TPU v7x, 32 devices: a whole 2x2x4 slice. The times are simulated.
32 devices in a mesh: conf: 2 (over y), res: 4 (over z), vec: 4 (over x, core).
Axes of the slice: x: 2, y: 2, z: 4, core: 2. Of those that a mesh axis runs over, the one named last changes fastest.
Arguments:
- start_block: float32 [256, 64, 128], P(('conf', 'res')), parts along dimension 0, may hold values from -6 to 6
- diagonal: float32 [256, 128], P(('conf', 'res')), parts along dimension 0, may hold values from 0.3 to 3
- hess_tiles: float32 [8, 4, 44, 128, 128], P(('conf', 'res'), 'vec'), parts along dimension 0, may hold values from -0.15625 to 0.15625
- tile_rows: int32 [8, 4, 44], P(('conf', 'res'), 'vec'), parts along dimension 0, may hold values from 0 to 31
- tile_cols: int32 [8, 4, 44], P(('conf', 'res'), 'vec'), parts along dimension 0, may hold values from 0 to 31
- slot_counts: int32 [8, 4, 3], P(('conf', 'res'), 'vec'), parts along dimension 0, may hold values from 0 to 8, as said below
Outputs:
- next_block: float32 [256, 64, 128], P(('conf', 'res')), parts along dimension 0
- coefficients: float32 [8, 64, 64], P('conf'), parts along dimension 0
There are 2 independent parts, one for each index of `conf`. A program takes and returns all parts, laid end to end along the dimension named above; each array names one. Nothing has to cross between parts.
Inputs may be any that keep to these rules, and one draw needn't show every extreme that they name: slot_counts[r, v, d - 1] is 0 exactly where r + d >= 4 and 1 or more elsewhere; for every hop d some shard has 8 on all of its devices.
All inputs are finite; a program needn't handle non-finite values.
Results may differ from a plain program's by a relative error of at most 0.0003.
Values sent between devices are 32-bit elements; how exact they have to be, the bound alone decides.
No kernel may reach another device: no remote copies, remote signals or barrier semaphores. Data moves between devices by JAX's collectives and lax.ppermute only.
A program may use at most 64 MiB of HBM per device.

v0:
```python
import math

import jax
import jax.numpy as jnp
from jax import lax
from jax.experimental import pallas as pl
from jax.experimental.pallas import tpu as pltpu
from jax.sharding import PartitionSpec as P

OWN_SLOTS = 20
HOPS = 3
CAP = 8
SHIFT = 1.65


def dot(a, b, ta=False, tb=False):
    dims = (((0 if ta else 1,), (1 if tb else 0,)), ((), ()))
    return lax.dot_general(
        a, b, dims, precision=lax.Precision.HIGHEST, preferred_element_type=jnp.float32
    )


VMEM = pl.BlockSpec(memory_space=pltpu.VMEM)
SMEM = pl.BlockSpec(memory_space=pltpu.SMEM)


def call(body, outs, in_specs, scratch=(), name=None):
    shapes = [jax.ShapeDtypeStruct(s, jnp.float32) for s in outs]
    return pl.pallas_call(
        body,
        out_shape=shapes,
        in_specs=in_specs,
        out_specs=[VMEM] * len(outs),
        scratch_shapes=list(scratch),
        compiler_params=pltpu.CompilerParams(vmem_limit_bytes=40 << 20),
        name=name,
    )


def pairings(size):
    rounds = []
    for hop in range(1, HOPS + 1):
        for parity in range(2):
            pairs = [
                (i, i + hop) for i in range(size - hop) if (i // hop) % 2 == parity
            ]
            if not pairs:
                continue
            used = {i for pair in pairs for i in pair}
            for entry in rounds:
                if not entry["used"] & used:
                    entry["used"] |= used
                    entry["pairs"] += pairs
                    entry["kinds"].append((hop, parity))
                    break
            else:
                rounds.append({"used": used, "pairs": pairs, "kinds": [(hop, parity)]})
    return rounds


def exchange(block, axis, pairs):
    return lax.ppermute(block, axis, [(a, b) for a, b in pairs] + [(b, a) for a, b in pairs])


def role_of(entry, rank, size):
    role = jnp.int32(0)
    for hop, parity in entry["kinds"]:
        lower = (rank + hop < size) & ((rank // hop) % 2 == parity)
        upper = (rank >= hop) & ((jnp.maximum(rank - hop, 0) // hop) % 2 == parity)
        role = jnp.where(lower, hop, jnp.where(upper, -hop, role))
    return role


def all_sum(block, axis):
    size = lax.axis_size(axis)
    if size & (size - 1):
        return lax.psum(block, axis)
    step = 1
    while step < size:
        masks = [step] if step * 2 >= size else [step, 2 * step, 3 * step]
        got = [
            lax.ppermute(block, axis, [(i, i ^ mask) for i in range(size)]) for mask in masks
        ]
        if len(got) == 1:
            block = block + got[0]
            step *= 2
        else:
            block = (block + got[0]) + (got[1] + got[2])
            step *= 4
    return block


def factor(gram):
    size = gram.shape[0]
    row_id = lax.broadcasted_iota(jnp.int32, (size, size), 0)
    col_id = lax.broadcasted_iota(jnp.int32, (size, size), 1)
    work = jnp.concatenate([gram, (row_id == col_id).astype(jnp.float32)], axis=1)
    blocks = [work[8 * b : 8 * b + 8] for b in range(size // 8)]
    sub = lax.broadcasted_iota(jnp.int32, (8, 2 * size), 0)
    for j in range(size):
        b, s = divmod(j, 8)
        row = blocks[b][s : s + 1]
        scaled = row / row[:, j : j + 1]
        scaled = jnp.broadcast_to(scaled, (8, 2 * size))
        for other in range(b, size // 8):
            col = jnp.broadcast_to(blocks[other][:, j : j + 1], (8, 2 * size))
            if other == b:
                col = jnp.where(sub > s, col, 0.0)
            blocks[other] = blocks[other] - col * scaled
    work = jnp.concatenate(blocks, axis=0)
    pivots = jnp.sum(jnp.where(row_id == col_id, work[:, :size], 0.0), axis=1, keepdims=True)
    work = work / jnp.sqrt(pivots)
    upper = jnp.where(col_id >= row_id, work[:, :size], 0.0)
    inverse = jnp.where(col_id <= row_id, work[:, size:], 0.0)
    return upper, inverse


def local(start_block, diagonal, hess_tiles, tile_rows, tile_cols, slot_counts):
    peers = lax.axis_size("res")
    lanes = lax.axis_size("vec")
    rows, width, length = start_block.shape
    half = rows // 2
    rounds = pairings(peers)
    count = len(rounds)
    full = (rows, width, length)
    halfshape = (half, width, length)
    packet = (CAP, width, length)
    square = (width, width)

    place = jnp.stack(
        [lax.axis_index("vec")]
        + [role_of(entry, lax.axis_index("res"), peers) for entry in rounds]
    ).astype(jnp.int32)

    asked = [exchange(tile_cols, "res", entry["pairs"]) for entry in rounds]

    def send_body(place_ref, rows_ref, counts_ref, *refs):
        asked_refs, (x_ref, tiles_ref), out_refs = refs[:count], refs[count : count + 2], refs[count + 2 :]
        for p in range(count):
            role = place_ref[1 + p]

            @pl.when(role > 0)
            def _():
                base = OWN_SLOTS + (role - 1) * CAP
                for c in range(CAP):
                    term = dot(x_ref[rows_ref[0, 0, base + c]], tiles_ref[0, 0, base + c])
                    out_refs[p][c] = jnp.where(c < counts_ref[0, 0, role - 1], term, 0.0)

            @pl.when(role < 0)
            def _():
                base = OWN_SLOTS + (-role - 1) * CAP
                for c in range(CAP):
                    out_refs[p][c] = x_ref[asked_refs[p][0, 0, base + c]]

            @pl.when(role == 0)
            def _():
                out_refs[p][...] = jnp.zeros(packet, jnp.float32)

    def own_body(place_ref, rows_ref, cols_ref, x_ref, diag_ref, tiles_ref, acc_ref):
        first = (place_ref[0] == 0).astype(jnp.float32)
        acc_ref[...] = x_ref[...] * ((diag_ref[...] - SHIFT) * first)[:, None, :]
        for s in range(OWN_SLOTS):
            i, j, tile = rows_ref[0, 0, s], cols_ref[0, 0, s], tiles_ref[0, 0, s]
            direct = dot(x_ref[j], tile, tb=True)
            mirror = dot(x_ref[i], tile)
            acc_ref[i] += direct
            acc_ref[j] += mirror

    def join_body(place_ref, rows_ref, counts_ref, *refs):
        asked_refs, got_refs = refs[:count], refs[count : 2 * count]
        tiles_ref, part_ref, keep_ref, give_ref, acc_ref = refs[2 * count :]
        acc_ref[...] = part_ref[...]
        for p in range(count):
            role = place_ref[1 + p]

            @pl.when(role > 0)
            def _():
                base = OWN_SLOTS + (role - 1) * CAP
                for c in range(CAP):
                    term = dot(got_refs[p][c], tiles_ref[0, 0, base + c], tb=True)
                    acc_ref[rows_ref[0, 0, base + c]] += jnp.where(
                        c < counts_ref[0, 0, role - 1], term, 0.0
                    )

            @pl.when(role < 0)
            def _():
                base = OWN_SLOTS + (-role - 1) * CAP
                for c in range(CAP):
                    acc_ref[asked_refs[p][0, 0, base + c]] += got_refs[p][c]

        core = place_ref[0] % 2
        keep_ref[...] = acc_ref[pl.ds(core * half, half)]
        give_ref[...] = acc_ref[pl.ds((1 - core) * half, half)]

    def gram_body(x_ref, out_ref):
        total = jnp.zeros(square, jnp.float32)
        for n in range(rows):
            total += dot(x_ref[n], x_ref[n], tb=True)
        out_ref[...] = total

    def settle_body(place_ref, mine_ref, other_ref, x_ref, y_ref, out_ref):
        core = place_ref[0] % 2
        y_ref[pl.ds(core * half, half)] = mine_ref[...]
        y_ref[pl.ds((1 - core) * half, half)] = other_ref[...]
        total = jnp.zeros((width, 2 * width), jnp.float32)
        for n in range(rows):
            y = y_ref[n]
            total += dot(y, jnp.concatenate([x_ref[n], y], axis=0), tb=True)
        out_ref[...] = total

    def first_body(gram_ref, inverse_ref):
        _, inverse_ref[...] = factor(gram_ref[...])

    def second_body(gram_ref, inverse_ref, cross_ref, lower_ref, coef_ref):
        start_inv = inverse_ref[...]
        cross = dot(dot(start_inv, gram_ref[:, :width]), start_inv, tb=True)
        applied = dot(dot(start_inv, gram_ref[:, width:]), start_inv, tb=True)
        upper, inverse = factor(applied - dot(cross, cross, tb=True))
        lower = upper.T
        eye = lax.broadcasted_iota(jnp.int32, square, 0) == lax.broadcasted_iota(jnp.int32, square, 1)
        cross_ref[...] = cross + jnp.where(eye, SHIFT, 0.0)
        lower_ref[...] = lower
        coef_ref[:, :width] = -dot(lower, start_inv)
        coef_ref[:, width : 2 * width] = -dot(dot(inverse, cross), start_inv)
        coef_ref[:, 2 * width :] = dot(inverse, start_inv)

    def third_body(place_ref, mine_ref, other_ref, x_ref, y_ref, coef_ref, w_ref, q_ref, out_ref, z_ref):
        core = place_ref[0] % 2
        z_ref[pl.ds(core * half, half)] = mine_ref[...]
        z_ref[pl.ds((1 - core) * half, half)] = other_ref[...]
        total = jnp.zeros((width, 2 * width), jnp.float32)
        for n in range(rows):
            stack = jnp.concatenate([x_ref[n], y_ref[n], z_ref[n]], axis=0)
            w = dot(coef_ref[...], stack)
            q = dot(coef_ref[:, width:], stack[: 2 * width])
            w_ref[n] = w
            q_ref[n] = q
            total += dot(w, jnp.concatenate([q, w], axis=0), tb=True)
        out_ref[...] = total

    def fourth_body(gram_ref, cross_ref, lower_ref, coef_ref):
        cross = gram_ref[:, :width]
        upper, inverse = factor(gram_ref[:, width:] - dot(cross, cross, tb=True))
        eye = lax.broadcasted_iota(jnp.int32, square, 0) == lax.broadcasted_iota(jnp.int32, square, 1)
        cross_ref[...] = cross + jnp.where(eye, SHIFT, 0.0)
        lower_ref[...] = upper.T
        scale = math.sqrt(rows * length * peers)
        coef_ref[:, :width] = inverse * scale
        coef_ref[:, width:] = -dot(inverse, cross) * scale

    def last_body(w_ref, q_ref, coef_ref, out_ref):
        for n in range(rows):
            out_ref[n] = dot(coef_ref[...], jnp.concatenate([w_ref[n], q_ref[n]], axis=0))

    def apply_shifted(x):
        sent = call(
            send_body, [packet] * count, [SMEM] * (3 + count) + [VMEM] * 2, name="send"
        )(place, tile_rows, slot_counts, *asked, x, hess_tiles)
        got = [exchange(s, "res", entry["pairs"]) for s, entry in zip(sent, rounds)]
        (part,) = call(own_body, [full], [SMEM] * 3 + [VMEM] * 3, name="own")(
            place, tile_rows, tile_cols, x, diagonal, hess_tiles
        )
        keep, give = call(
            join_body,
            [halfshape] * 2,
            [SMEM] * (3 + count) + [VMEM] * (count + 2),
            [pltpu.VMEM(full, jnp.float32)],
            name="join",
        )(place, tile_rows, slot_counts, *asked, *got, hess_tiles, part)
        swap = [(i, i ^ 1) for i in range(lanes)]
        mine = keep + lax.ppermute(give, "vec", swap)
        step = 2
        while step < lanes:
            mine = mine + lax.ppermute(mine, "vec", [(i, i ^ step) for i in range(lanes)])
            step *= 2
        return mine, lax.ppermute(mine, "vec", swap)

    (start_gram,) = call(gram_body, [square], [VMEM], name="gram")(start_block)
    start_gram = all_sum(start_gram, "res")
    (start_inv,) = call(first_body, [square], [VMEM], name="first")(start_gram)

    mine, other = apply_shifted(start_block)
    y, gram = call(settle_body, [full, (width, 2 * width)], [SMEM] + [VMEM] * 3, name="settle")(
        place, mine, other, start_block
    )
    gram = all_sum(gram, "res")
    cross1, lower1, coef = call(
        second_body, [square, square, (width, 3 * width)], [VMEM] * 2, name="second"
    )(gram, start_inv)
    mine, other = apply_shifted(y)
    w, q, gram = call(
        third_body,
        [full, full, (width, 2 * width)],
        [SMEM] + [VMEM] * 5,
        [pltpu.VMEM(full, jnp.float32)],
        name="third",
    )(place, mine, other, start_block, y, coef)
    gram = all_sum(gram, "res")
    cross2, lower2, coef = call(
        fourth_body, [square, square, (width, 2 * width)], [VMEM], name="fourth"
    )(gram)
    (next_block,) = call(last_body, [full], [VMEM] * 3, name="last")(w, q, coef)
    return next_block, jnp.stack([cross1, lower1, cross2, lower2])


def solution(mesh):
    in_specs = (
        P(("conf", "res"), None, None),
        P(("conf", "res"), None),
        P(("conf", "res"), "vec", None, None, None),
        P(("conf", "res"), "vec", None),
        P(("conf", "res"), "vec", None),
        P(("conf", "res"), "vec", None),
    )
    out_specs = (P(("conf", "res"), None, None), P("conf", None, None))
    return jax.shard_map(local, mesh=mesh, in_specs=in_specs, out_specs=out_specs, check_vma=False)
```

profile of v0, /device:TPU:0, one launch (start us, length us, event | category | flops | bytes accessed | tf_op | source)
XLA Modules:
  0.0 166.3 jit_solution(5968590452963531773)
XLA Ops:
  0.6 4.1 %collective-permute-start.2 = (s32[1,1,44]{2,1,0:T(1,128)}, s32[1,1,44]{2,1,0:T(1,128)S(1)}, u32[]{:S(2)}, u32[]{:S(2)}) collective-permute-start(s32[1,1,44]{2,1,0:T(1,128)} %cols_ref.3), channel_id=1, source_target_pairs={{0,8},{4,12},{8,0},{12,4},{1,9},{5,13},{9,1},{13,5},{2,10},{6,14},... | collective-permute-start | bytes 536 | tf_op jit(solution)/shard_map/ppermute | solution.py:62
  6.4 3.8 %collective-permute-done.1.refs_1_ = s32[1,1,44]{2,1,0:T(1,128)S(1)} collective-permute-done((s32[1,1,44]{2,1,0:T(1,128)}, s32[1,1,44]{2,1,0:T(1,128)S(1)}, u32[]{:S(2)}, u32[]{:S(2)}) %collective-permute-start.1) | collective-permute-done | bytes 208 | tf_op jit(solution)/shard_map/ppermute | solution.py:62
  10.2 1.8 %copy-done = f32[1,1,44,128,128]{4,3,2,1,0:T(8,128)S(1)} copy-done((f32[1,1,44,128,128]{4,3,2,1,0:T(8,128)S(1)}, f32[1,1,44,128,128]{4,3,2,1,0:T(8,128)}, u32[]{:S(2)}) %copy-start) | copy-done | bytes 2883608
  14.6 2.3 %send.2 = (f32[8,64,128]{2,1,0:T(8,128)S(1)}, f32[8,64,128]{2,1,0:T(8,128)S(1)}, f32[8,64,128]{2,1,0:T(8,128)S(1)}) custom-call(s32[4]{0:T(128)S(1)} %pad_add_fusion.place_ref, s32[1,1,44]{2,1,0:T(1,128)S(1)} %copy-done.5, s32[1,1,3]{2,1,0:T(1,128)S(1)} %copy-done.6, s32[1,1,44]{2,1,0:T(1,128)S(1)} %collective-permute-done.refs_0_, ...), custom_call_target="tpu_custom_call" | custom-call | tf_op jit(solution)/shard_map/send/pallas_call | solution.py:256
  18.6 1.9 %collective-permute-start.5 = (f32[8,64,128]{2,1,0:T(8,128)S(1)}, f32[8,64,128]{2,1,0:T(8,128)S(1)}, u32[]{:S(2)}, u32[]{:S(2)}) collective-permute-start(f32[8,64,128]{2,1,0:T(8,128)S(1)} %get-tuple-element.25), channel_id=1, source_target_pairs={{0,8},{4,12},{8,0},{12,4},{1,9},{5,13},{9,1},{13,5},{2,10},{6,14},... | collective-permute-start | bytes 786440 | tf_op jit(solution)/shard_map/ppermute | solution.py:62
  20.4 4.0 %own.2.refs_7_ = f32[32,64,128]{2,1,0:T(8,128)S(1)} custom-call(s32[4]{0:T(128)S(1)} %pad_add_fusion.place_ref, s32[1,1,44]{2,1,0:T(1,128)S(1)} %copy-done.5, s32[1,1,44]{2,1,0:T(1,128)S(1)} %copy-done.8, f32[32,64,128]{2,1,0:T(8,128)S(1)} %copy-done.2, f32[32,128]{1,0:T(8,128)S(1)} %copy-done.4, f32[1,1,44,128,128]{4,3,2,1,0:T(8,128)S(1)} %copy-done.1), custom_call_target="tpu_custom_call" | custom-call | tf_op jit(solution)/shard_map/own/pallas_call | solution.py:260
  24.4 2.6 %collective-permute-done.3.refs_3_ = f32[8,64,128]{2,1,0:T(8,128)S(1)} collective-permute-done((f32[8,64,128]{2,1,0:T(8,128)S(1)}, f32[8,64,128]{2,1,0:T(8,128)S(1)}, u32[]{:S(2)}, u32[]{:S(2)}) %collective-permute-start.3) | collective-permute-done | bytes 262176 | tf_op jit(solution)/shard_map/ppermute | solution.py:62
  27.0 4.3 %collective-permute-done.4.refs_4_ = f32[8,64,128]{2,1,0:T(8,128)S(1)} collective-permute-done((f32[8,64,128]{2,1,0:T(8,128)S(1)}, f32[8,64,128]{2,1,0:T(8,128)S(1)}, u32[]{:S(2)}, u32[]{:S(2)}) %collective-permute-start.4) | collective-permute-done | bytes 262176 | tf_op jit(solution)/shard_map/ppermute | solution.py:62
  31.3 10.3 %collective-permute-done.5.refs_5_ = f32[8,64,128]{2,1,0:T(8,128)S(1)} collective-permute-done((f32[8,64,128]{2,1,0:T(8,128)S(1)}, f32[8,64,128]{2,1,0:T(8,128)S(1)}, u32[]{:S(2)}, u32[]{:S(2)}) %collective-permute-start.5) | collective-permute-done | bytes 262176 | tf_op jit(solution)/shard_map/ppermute | solution.py:62
  41.6 4.1 %join.2 = (f32[16,64,128]{2,1,0:T(8,128)S(1)}, f32[16,64,128]{2,1,0:T(8,128)S(1)}) custom-call(s32[4]{0:T(128)S(1)} %pad_add_fusion.place_ref, s32[1,1,44]{2,1,0:T(1,128)S(1)} %copy-done.5, s32[1,1,3]{2,1,0:T(1,128)S(1)} %copy-done.6, s32[1,1,44]{2,1,0:T(1,128)S(1)} %collective-permute-done.refs_0_, s32[1,1,44]{2,1,0:T(1,128)S(1)} %collective-permute-done.1.refs_1_, ...), custom_call_target="tpu_custom_call" | custom-call | tf_op jit(solution)/shard_map/join/pallas_call | solution.py:263
  45.8 1.9 %collective-permute-done.6 = f32[16,64,128]{2,1,0:T(8,128)S(1)} collective-permute-done((f32[16,64,128]{2,1,0:T(8,128)S(1)}, f32[16,64,128]{2,1,0:T(8,128)S(1)}, u32[]{:S(2)}, u32[]{:S(2)}) %collective-permute-start.6) | collective-permute-done | bytes 524320 | tf_op jit(solution)/shard_map/ppermute | solution.py:271
  49.3 12.5 %collective-permute-done.7 = f32[16,64,128]{2,1,0:T(8,128)S(1)} collective-permute-done((f32[16,64,128]{2,1,0:T(8,128)S(1)}, f32[16,64,128]{2,1,0:T(8,128)S(1)}, u32[]{:S(2)}, u32[]{:S(2)}) %collective-permute-start.7) | collective-permute-done | bytes 524320 | tf_op jit(solution)/shard_map/ppermute | solution.py:274
  61.9 1.9 %collective-permute-done.8.other_ref = f32[16,64,128]{2,1,0:T(8,128)S(1)} collective-permute-done((f32[16,64,128]{2,1,0:T(8,128)S(1)}, f32[16,64,128]{2,1,0:T(8,128)S(1)}, u32[]{:S(2)}, u32[]{:S(2)}) %collective-permute-start.8) | collective-permute-done | bytes 524320 | tf_op jit(solution)/shard_map/ppermute | solution.py:276
  63.8 4.6 %settle.1 = (f32[32,64,128]{2,1,0:T(8,128)S(1)}, f32[64,128]{1,0:T(8,128)S(1)}) custom-call(s32[4]{0:T(128)S(1)} %pad_add_fusion.place_ref, f32[16,64,128]{2,1,0:T(8,128)S(1)} %add.89.mine_ref, f32[16,64,128]{2,1,0:T(8,128)S(1)} %collective-permute-done.8.other_ref, f32[32,64,128]{2,1,0:T(8,128)S(1)} %copy-done.3), custom_call_target="tpu_custom_call" | custom-call | tf_op jit(solution)/shard_map/settle/pallas_call | solution.py:283
  68.4 2.4 %send.3 = (f32[8,64,128]{2,1,0:T(8,128)S(1)}, f32[8,64,128]{2,1,0:T(8,128)S(1)}, f32[8,64,128]{2,1,0:T(8,128)S(1)}) custom-call(s32[4]{0:T(128)S(1)} %pad_add_fusion.place_ref, s32[1,1,44]{2,1,0:T(1,128)S(1)} %copy-done.5, s32[1,1,3]{2,1,0:T(1,128)S(1)} %copy-done.7, s32[1,1,44]{2,1,0:T(1,128)S(1)} %collective-permute-done.refs_0_, ...), custom_call_target="tpu_custom_call" | custom-call | tf_op jit(solution)/shard_map/send/pallas_call | solution.py:256
  71.0 3.4 %collective-permute-start.11 = (f32[8,64,128]{2,1,0:T(8,128)S(1)}, f32[8,64,128]{2,1,0:T(8,128)S(1)}, u32[]{:S(2)}, u32[]{:S(2)}) collective-permute-start(f32[8,64,128]{2,1,0:T(8,128)S(1)} %get-tuple-element.31), channel_id=1, source_target_pairs={{0,8},{4,12},{8,0},{12,4},{1,9},{5,13},{9,1},{13,5},{2,10},{6,14},... | collective-permute-start | bytes 786440 | tf_op jit(solution)/shard_map/ppermute | solution.py:62
  74.4 4.0 %own.3.refs_7_ = f32[32,64,128]{2,1,0:T(8,128)S(1)} custom-call(s32[4]{0:T(128)S(1)} %pad_add_fusion.place_ref, s32[1,1,44]{2,1,0:T(1,128)S(1)} %copy-done.5, s32[1,1,44]{2,1,0:T(1,128)S(1)} %copy-done.8, f32[32,64,128]{2,1,0:T(8,128)S(1)} %get-tuple-element.28.refs_3_.x_ref.y_ref, f32[32,128]{1,0:T(8,128)S(1)} %copy-done.4, ...), custom_call_target="tpu_custom_call" | custom-call | tf_op jit(solution)/shard_map/own/pallas_call | solution.py:260
  78.4 6.5 %collective-permute-done.9.refs_3_ = f32[8,64,128]{2,1,0:T(8,128)S(1)} collective-permute-done((f32[8,64,128]{2,1,0:T(8,128)S(1)}, f32[8,64,128]{2,1,0:T(8,128)S(1)}, u32[]{:S(2)}, u32[]{:S(2)}) %collective-permute-start.9) | collective-permute-done | bytes 262176 | tf_op jit(solution)/shard_map/ppermute | solution.py:62
  84.9 12.4 %collective-permute-done.11.refs_5_ = f32[8,64,128]{2,1,0:T(8,128)S(1)} collective-permute-done((f32[8,64,128]{2,1,0:T(8,128)S(1)}, f32[8,64,128]{2,1,0:T(8,128)S(1)}, u32[]{:S(2)}, u32[]{:S(2)}) %collective-permute-start.11) | collective-permute-done | bytes 262176 | tf_op jit(solution)/shard_map/ppermute | solution.py:62
  97.3 4.1 %join.3 = (f32[16,64,128]{2,1,0:T(8,128)S(1)}, f32[16,64,128]{2,1,0:T(8,128)S(1)}) custom-call(s32[4]{0:T(128)S(1)} %pad_add_fusion.place_ref, s32[1,1,44]{2,1,0:T(1,128)S(1)} %copy-done.5, s32[1,1,3]{2,1,0:T(1,128)S(1)} %copy-done.7, s32[1,1,44]{2,1,0:T(1,128)S(1)} %collective-permute-done.refs_0_, s32[1,1,44]{2,1,0:T(1,128)S(1)} %collective-permute-done.1.refs_1_, ...), custom_call_target="tpu_custom_call" | custom-call | tf_op jit(solution)/shard_map/join/pallas_call | solution.py:263
  101.5 1.9 %collective-permute-done.12 = f32[16,64,128]{2,1,0:T(8,128)S(1)} collective-permute-done((f32[16,64,128]{2,1,0:T(8,128)S(1)}, f32[16,64,128]{2,1,0:T(8,128)S(1)}, u32[]{:S(2)}, u32[]{:S(2)}) %collective-permute-start.12) | collective-permute-done | bytes 524320 | tf_op jit(solution)/shard_map/ppermute | solution.py:271
  105.0 12.5 %collective-permute-done.13 = f32[16,64,128]{2,1,0:T(8,128)S(1)} collective-permute-done((f32[16,64,128]{2,1,0:T(8,128)S(1)}, f32[16,64,128]{2,1,0:T(8,128)S(1)}, u32[]{:S(2)}, u32[]{:S(2)}) %collective-permute-start.13) | collective-permute-done | bytes 524320 | tf_op jit(solution)/shard_map/ppermute | solution.py:274
  117.6 1.7 %gram.1 = f32[64,64]{1,0:T(8,128)S(1)} custom-call(f32[32,64,128]{2,1,0:T(8,128)S(1)} %copy-done.3), custom_call_target="tpu_custom_call" | custom-call | tf_op jit(solution)/shard_map/gram/pallas_call | solution.py:278
  119.5 4.3 %collective-permute-start.18 = (f32[64,64]{1,0:T(8,128)S(1)}, f32[64,64]{1,0:T(8,128)S(1)}, u32[]{:S(2)}, u32[]{:S(2)}) collective-permute-start(f32[64,64]{1,0:T(8,128)S(1)} %gram.1), channel_id=1, source_target_pairs={{0,4},{4,0},{8,12},{12,8},{1,5},{5,1},{9,13},{13,9},{2,6},{6,2},{1... | collective-permute-start | bytes 49160 | tf_op jit(solution)/shard_map/ppermute | solution.py:82
  125.4 2.8 %collective-permute-start.15 = (f32[64,128]{1,0:T(8,128)S(1)}, f32[64,128]{1,0:T(8,128)S(1)}, u32[]{:S(2)}, u32[]{:S(2)}) collective-permute-start(f32[64,128]{1,0:T(8,128)S(1)} %get-tuple-element.34), channel_id=1, source_target_pairs={{0,4},{4,0},{8,12},{12,8},{1,5},{5,1},{9,13},{13,9},{2,6},{6,2},{1... | collective-permute-start | bytes 98312 | tf_op jit(solution)/shard_map/ppermute | solution.py:82
  128.2 5.5 %first.1.inverse_ref = f32[64,64]{1,0:T(8,128)S(1)} custom-call(f32[64,64]{1,0:T(8,128)S(1)} %add_add_fusion.1.gram_ref), custom_call_target="tpu_custom_call" | custom-call | tf_op jit(solution)/shard_map/first/pallas_call | solution.py:280
  133.8 6.5 %second.1 = (f32[64,64]{1,0:T(8,128)S(1)}, f32[64,64]{1,0:T(8,128)S(1)}, f32[64,192]{1,0:T(8,128)S(1)}) custom-call(f32[64,128]{1,0:T(8,128)S(1)} %add_add_fusion.2.gram_ref, f32[64,64]{1,0:T(8,128)S(1)} %first.1.inverse_ref), custom_call_target="tpu_custom_call" | custom-call | tf_op jit(solution)/shard_map/second/pallas_call | solution.py:287
  140.3 9.8 %third.1 = (f32[32,64,128]{2,1,0:T(8,128)S(1)}, f32[32,64,128]{2,1,0:T(8,128)S(1)}, f32[64,128]{1,0:T(8,128)S(1)}) custom-call(s32[4]{0:T(128)S(1)} %pad_add_fusion.place_ref, f32[16,64,128]{2,1,0:T(8,128)S(1)} %add.91.mine_ref, f32[16,64,128]{2,1,0:T(8,128)S(1)} %collective-permute-done.14.other_ref, f32[32,64,128]{2,1,0:T(8,128)S(1)} %copy-done.3, ...), custom_call_target="tpu_custom_call" | custom-call | tf_op jit(solution)/shard_map/third/pallas_call | solution.py:291
  150.1 1.7 collective-permute-start.23
  151.8 2.8 %collective-permute-start.21 = (f32[64,128]{1,0:T(8,128)S(1)}, f32[64,128]{1,0:T(8,128)S(1)}, u32[]{:S(2)}, u32[]{:S(2)}) collective-permute-start(f32[64,128]{1,0:T(8,128)S(1)} %get-tuple-element.38), channel_id=1, source_target_pairs={{0,4},{4,0},{8,12},{12,8},{1,5},{5,1},{9,13},{13,9},{2,6},{6,2},{1... | collective-permute-start | bytes 98312 | tf_op jit(solution)/shard_map/ppermute | solution.py:82
  156.8 6.1 %fourth.1 = (f32[64,64]{1,0:T(8,128)S(1)}, f32[64,64]{1,0:T(8,128)S(1)}, f32[64,128]{1,0:T(8,128)S(1)}) custom-call(f32[64,128]{1,0:T(8,128)S(1)} %add_add_fusion.gram_ref), custom_call_target="tpu_custom_call" | custom-call | tf_op jit(solution)/shard_map/fourth/pallas_call | solution.py:299
  162.9 2.8 %last.1 = f32[32,64,128]{2,1,0:T(8,128)} custom-call(f32[32,64,128]{2,1,0:T(8,128)S(1)} %get-tuple-element.36.w_ref, f32[32,64,128]{2,1,0:T(8,128)S(1)} %get-tuple-element.37.q_ref, f32[64,128]{1,0:T(8,128)S(1)} %get-tuple-element.39.coef_ref), custom_call_target="tpu_custom_call" | custom-call | tf_op jit(solution)/shard_map/last/pallas_call | solution.py:302
  (56 shorter events, 14.4 us)
Async XLA Ops:
  0.6 19.8 %copy-start.8 = (s32[1,1,44]{2,1,0:T(1,128)S(1)}, s32[1,1,44]{2,1,0:T(1,128)}, u32[]{:S(2)}) copy-start(s32[1,1,44]{2,1,0:T(1,128)} %cols_ref.3) | copy-start | bytes 532
  0.6 19.8 %copy-start.4 = (f32[32,128]{1,0:T(8,128)S(1)}, f32[32,128]{1,0:T(8,128)}, u32[]{:S(2)}) copy-start(f32[32,128]{1,0:T(8,128)} %diag_ref.3) | copy-start | bytes 49156
  0.6 5.8 %collective-permute-start.2 = (s32[1,1,44]{2,1,0:T(1,128)}, s32[1,1,44]{2,1,0:T(1,128)S(1)}, u32[]{:S(2)}, u32[]{:S(2)}) collective-permute-start(s32[1,1,44]{2,1,0:T(1,128)} %cols_ref.3), channel_id=1, source_target_pairs={{0,8},{4,12},{8,0},{12,4},{1,9},{5,13},{9,1},{13,5},{2,10},{6,14},... | collective-permute-start | bytes 536 | tf_op jit(solution)/shard_map/ppermute | solution.py:62
  4.8 5.5 %collective-permute-start.1 = (s32[1,1,44]{2,1,0:T(1,128)}, s32[1,1,44]{2,1,0:T(1,128)S(1)}, u32[]{:S(2)}, u32[]{:S(2)}) collective-permute-start(s32[1,1,44]{2,1,0:T(1,128)} %cols_ref.3), channel_id=1, source_target_pairs={{4,8},{0,12},{8,4},{12,0},{5,9},{1,13},{9,5},{13,1},{6,10},{2,14},... | collective-permute-start | bytes 536 | tf_op jit(solution)/shard_map/ppermute | solution.py:62
  6.1 4.1 %collective-permute-start = (s32[1,1,44]{2,1,0:T(1,128)}, s32[1,1,44]{2,1,0:T(1,128)S(1)}, u32[]{:S(2)}, u32[]{:S(2)}) collective-permute-start(s32[1,1,44]{2,1,0:T(1,128)} %cols_ref.3), channel_id=1, source_target_pairs={{0,4},{8,12},{4,0},{12,8},{1,5},{9,13},{5,1},{13,9},{2,6},{10,14},... | collective-permute-start | bytes 536 | tf_op jit(solution)/shard_map/ppermute | solution.py:62
  10.2 1.8 %copy-start = (f32[1,1,44,128,128]{4,3,2,1,0:T(8,128)S(1)}, f32[1,1,44,128,128]{4,3,2,1,0:T(8,128)}, u32[]{:S(2)}) copy-start(f32[1,1,44,128,128]{4,3,2,1,0:T(8,128)} %refs_6_.3) | copy-start | bytes 8650756
  12.0 1.2 copy-start.2
  13.3 0.7 copy-start.5
  14.6 5.8 %copy-start.1 = (f32[1,1,44,128,128]{4,3,2,1,0:T(8,128)S(1)}, f32[1,1,44,128,128]{4,3,2,1,0:T(8,128)}, u32[]{:S(2)}) copy-start(f32[1,1,44,128,128]{4,3,2,1,0:T(8,128)} %refs_6_.3) | copy-start | bytes 8650756
  16.9 10.1 %collective-permute-start.3 = (f32[8,64,128]{2,1,0:T(8,128)S(1)}, f32[8,64,128]{2,1,0:T(8,128)S(1)}, u32[]{:S(2)}, u32[]{:S(2)}) collective-permute-start(f32[8,64,128]{2,1,0:T(8,128)S(1)} %get-tuple-element.23), channel_id=1, source_target_pairs={{0,4},{8,12},{4,0},{12,8},{1,5},{9,13},{5,1},{13,9},{2,6},{10,14},... | collective-permute-start | bytes 786440 | tf_op jit(solution)/shard_map/ppermute | solution.py:62
  16.9 14.4 %collective-permute-start.4 = (f32[8,64,128]{2,1,0:T(8,128)S(1)}, f32[8,64,128]{2,1,0:T(8,128)S(1)}, u32[]{:S(2)}, u32[]{:S(2)}) collective-permute-start(f32[8,64,128]{2,1,0:T(8,128)S(1)} %get-tuple-element.24), channel_id=1, source_target_pairs={{4,8},{0,12},{8,4},{12,0},{5,9},{1,13},{9,5},{13,1},{6,10},{2,14},... | collective-permute-start | bytes 786440 | tf_op jit(solution)/shard_map/ppermute | solution.py:62
  18.6 23.0 %collective-permute-start.5 = (f32[8,64,128]{2,1,0:T(8,128)S(1)}, f32[8,64,128]{2,1,0:T(8,128)S(1)}, u32[]{:S(2)}, u32[]{:S(2)}) collective-permute-start(f32[8,64,128]{2,1,0:T(8,128)S(1)} %get-tuple-element.25), channel_id=1, source_target_pairs={{0,8},{4,12},{8,0},{12,4},{1,9},{5,13},{9,1},{13,5},{2,10},{6,14},... | collective-permute-start | bytes 786440 | tf_op jit(solution)/shard_map/ppermute | solution.py:62
  24.4 39.4 %copy-start.3 = (f32[32,64,128]{2,1,0:T(8,128)S(1)}, f32[32,64,128]{2,1,0:T(8,128)}, u32[]{:S(2)}) copy-start(f32[32,64,128]{2,1,0:T(8,128)} %x_ref.7) | copy-start | bytes 3145732
  45.7 22.7 %copy-start.7 = (s32[1,1,3]{2,1,0:T(1,128)S(1)}, s32[1,1,3]{2,1,0:T(1,128)}, u32[]{:S(2)}) copy-start(s32[1,1,3]{2,1,0:T(1,128)} %counts_ref.7) | copy-start | bytes 40
  45.7 2.0 %collective-permute-start.6 = (f32[16,64,128]{2,1,0:T(8,128)S(1)}, f32[16,64,128]{2,1,0:T(8,128)S(1)}, u32[]{:S(2)}, u32[]{:S(2)}) collective-permute-start(f32[16,64,128]{2,1,0:T(8,128)S(1)} %get-tuple-element.27), channel_id=1, source_target_pairs={{0,1},{1,0},{2,3},{3,2},{4,5},{5,4},{6,7},{7,6},{8,9},{9,8},{10,11... | collective-permute-start | bytes 1572872 | tf_op jit(solution)/shard_map/ppermute | solution.py:271
  47.7 14.0 %collective-permute-start.7 = (f32[16,64,128]{2,1,0:T(8,128)S(1)}, f32[16,64,128]{2,1,0:T(8,128)S(1)}, u32[]{:S(2)}, u32[]{:S(2)}) collective-permute-start(f32[16,64,128]{2,1,0:T(8,128)S(1)} %add.88), channel_id=1, source_target_pairs={{0,2},{1,3},{2,0},{3,1},{4,6},{5,7},{6,4},{7,5},{8,10},{9,11},{10,... | collective-permute-start | bytes 1572872 | tf_op jit(solution)/shard_map/ppermute | solution.py:274
  61.8 2.0 %collective-permute-start.8 = (f32[16,64,128]{2,1,0:T(8,128)S(1)}, f32[16,64,128]{2,1,0:T(8,128)S(1)}, u32[]{:S(2)}, u32[]{:S(2)}) collective-permute-start(f32[16,64,128]{2,1,0:T(8,128)S(1)} %add.89.mine_ref), channel_id=1, source_target_pairs={{0,1},{1,0},{2,3},{3,2},{4,5},{5,4},{6,7},{7,6},{8,9},{9,8},{10,11... | collective-permute-start | bytes 1572872 | tf_op jit(solution)/shard_map/ppermute | solution.py:276
  70.8 14.0 %collective-permute-start.9 = (f32[8,64,128]{2,1,0:T(8,128)S(1)}, f32[8,64,128]{2,1,0:T(8,128)S(1)}, u32[]{:S(2)}, u32[]{:S(2)}) collective-permute-start(f32[8,64,128]{2,1,0:T(8,128)S(1)} %get-tuple-element.29), channel_id=1, source_target_pairs={{0,4},{8,12},{4,0},{12,8},{1,5},{9,13},{5,1},{13,9},{2,6},{10,14},... | collective-permute-start | bytes 786440 | tf_op jit(solution)/shard_map/ppermute | solution.py:62
  70.9 14.0 %collective-permute-start.10 = (f32[8,64,128]{2,1,0:T(8,128)S(1)}, f32[8,64,128]{2,1,0:T(8,128)S(1)}, u32[]{:S(2)}, u32[]{:S(2)}) collective-permute-start(f32[8,64,128]{2,1,0:T(8,128)S(1)} %get-tuple-element.30), channel_id=1, source_target_pairs={{4,8},{0,12},{8,4},{12,0},{5,9},{1,13},{9,5},{13,1},{6,10},{2,14},... | collective-permute-start | bytes 786440 | tf_op jit(solution)/shard_map/ppermute | solution.py:62
  71.0 26.3 %collective-permute-start.11 = (f32[8,64,128]{2,1,0:T(8,128)S(1)}, f32[8,64,128]{2,1,0:T(8,128)S(1)}, u32[]{:S(2)}, u32[]{:S(2)}) collective-permute-start(f32[8,64,128]{2,1,0:T(8,128)S(1)} %get-tuple-element.31), channel_id=1, source_target_pairs={{0,8},{4,12},{8,0},{12,4},{1,9},{5,13},{9,1},{13,5},{2,10},{6,14},... | collective-permute-start | bytes 786440 | tf_op jit(solution)/shard_map/ppermute | solution.py:62
  101.4 2.0 %collective-permute-start.12 = (f32[16,64,128]{2,1,0:T(8,128)S(1)}, f32[16,64,128]{2,1,0:T(8,128)S(1)}, u32[]{:S(2)}, u32[]{:S(2)}) collective-permute-start(f32[16,64,128]{2,1,0:T(8,128)S(1)} %get-tuple-element.33), channel_id=1, source_target_pairs={{0,1},{1,0},{2,3},{3,2},{4,5},{5,4},{6,7},{7,6},{8,9},{9,8},{10,11... | collective-permute-start | bytes 1572872 | tf_op jit(solution)/shard_map/ppermute | solution.py:271
  103.5 14.0 %collective-permute-start.13 = (f32[16,64,128]{2,1,0:T(8,128)S(1)}, f32[16,64,128]{2,1,0:T(8,128)S(1)}, u32[]{:S(2)}, u32[]{:S(2)}) collective-permute-start(f32[16,64,128]{2,1,0:T(8,128)S(1)} %add.90), channel_id=1, source_target_pairs={{0,2},{1,3},{2,0},{3,1},{4,6},{5,7},{6,4},{7,5},{8,10},{9,11},{10,... | collective-permute-start | bytes 1572872 | tf_op jit(solution)/shard_map/ppermute | solution.py:274
  117.6 22.7 %collective-permute-start.14 = (f32[16,64,128]{2,1,0:T(8,128)S(1)}, f32[16,64,128]{2,1,0:T(8,128)S(1)}, u32[]{:S(2)}, u32[]{:S(2)}) collective-permute-start(f32[16,64,128]{2,1,0:T(8,128)S(1)} %add.91.mine_ref), channel_id=1, source_target_pairs={{0,1},{1,0},{2,3},{3,2},{4,5},{5,4},{6,7},{7,6},{8,9},{9,8},{10,11... | collective-permute-start | bytes 1572872 | tf_op jit(solution)/shard_map/ppermute | solution.py:276
  119.4 6.0 %collective-permute-start.20 = (f32[64,64]{1,0:T(8,128)S(1)}, f32[64,64]{1,0:T(8,128)S(1)}, u32[]{:S(2)}, u32[]{:S(2)}) collective-permute-start(f32[64,64]{1,0:T(8,128)S(1)} %gram.1), channel_id=1, source_target_pairs={{0,12},{4,8},{8,4},{12,0},{1,13},{5,9},{9,5},{13,1},{2,14},{6,10},... | collective-permute-start | bytes 49160 | tf_op jit(solution)/shard_map/ppermute | solution.py:82
  119.5 6.0 %collective-permute-start.19 = (f32[64,64]{1,0:T(8,128)S(1)}, f32[64,64]{1,0:T(8,128)S(1)}, u32[]{:S(2)}, u32[]{:S(2)}) collective-permute-start(f32[64,64]{1,0:T(8,128)S(1)} %gram.1), channel_id=1, source_target_pairs={{0,8},{4,12},{8,0},{12,4},{1,9},{5,13},{9,1},{13,5},{2,10},{6,14},... | collective-permute-start | bytes 49160 | tf_op jit(solution)/shard_map/ppermute | solution.py:82
  119.5 8.7 %collective-permute-start.18 = (f32[64,64]{1,0:T(8,128)S(1)}, f32[64,64]{1,0:T(8,128)S(1)}, u32[]{:S(2)}, u32[]{:S(2)}) collective-permute-start(f32[64,64]{1,0:T(8,128)S(1)} %gram.1), channel_id=1, source_target_pairs={{0,4},{4,0},{8,12},{12,8},{1,5},{5,1},{9,13},{13,9},{2,6},{6,2},{1... | collective-permute-start | bytes 49160 | tf_op jit(solution)/shard_map/ppermute | solution.py:82
  123.8 9.9 %collective-permute-start.17 = (f32[64,128]{1,0:T(8,128)S(1)}, f32[64,128]{1,0:T(8,128)S(1)}, u32[]{:S(2)}, u32[]{:S(2)}) collective-permute-start(f32[64,128]{1,0:T(8,128)S(1)} %get-tuple-element.34), channel_id=1, source_target_pairs={{0,12},{4,8},{8,4},{12,0},{1,13},{5,9},{9,5},{13,1},{2,14},{6,10},... | collective-permute-start | bytes 98312 | tf_op jit(solution)/shard_map/ppermute | solution.py:82
  125.4 8.4 %collective-permute-start.16 = (f32[64,128]{1,0:T(8,128)S(1)}, f32[64,128]{1,0:T(8,128)S(1)}, u32[]{:S(2)}, u32[]{:S(2)}) collective-permute-start(f32[64,128]{1,0:T(8,128)S(1)} %get-tuple-element.34), channel_id=1, source_target_pairs={{0,8},{4,12},{8,0},{12,4},{1,9},{5,13},{9,1},{13,5},{2,10},{6,14},... | collective-permute-start | bytes 98312 | tf_op jit(solution)/shard_map/ppermute | solution.py:82
  125.4 8.4 %collective-permute-start.15 = (f32[64,128]{1,0:T(8,128)S(1)}, f32[64,128]{1,0:T(8,128)S(1)}, u32[]{:S(2)}, u32[]{:S(2)}) collective-permute-start(f32[64,128]{1,0:T(8,128)S(1)} %get-tuple-element.34), channel_id=1, source_target_pairs={{0,4},{4,0},{8,12},{12,8},{1,5},{5,1},{9,13},{13,9},{2,6},{6,2},{1... | collective-permute-start | bytes 98312 | tf_op jit(solution)/shard_map/ppermute | solution.py:82
  150.1 5.8 %collective-permute-start.23 = (f32[64,128]{1,0:T(8,128)S(1)}, f32[64,128]{1,0:T(8,128)S(1)}, u32[]{:S(2)}, u32[]{:S(2)}) collective-permute-start(f32[64,128]{1,0:T(8,128)S(1)} %get-tuple-element.38), channel_id=1, source_target_pairs={{0,12},{4,8},{8,4},{12,0},{1,13},{5,9},{9,5},{13,1},{2,14},{6,10},... | collective-permute-start | bytes 98312 | tf_op jit(solution)/shard_map/ppermute | solution.py:82
  151.8 4.9 %collective-permute-start.22 = (f32[64,128]{1,0:T(8,128)S(1)}, f32[64,128]{1,0:T(8,128)S(1)}, u32[]{:S(2)}, u32[]{:S(2)}) collective-permute-start(f32[64,128]{1,0:T(8,128)S(1)} %get-tuple-element.38), channel_id=1, source_target_pairs={{0,8},{4,12},{8,0},{12,4},{1,9},{5,13},{9,1},{13,5},{2,10},{6,14},... | collective-permute-start | bytes 98312 | tf_op jit(solution)/shard_map/ppermute | solution.py:82
  151.8 5.0 %collective-permute-start.21 = (f32[64,128]{1,0:T(8,128)S(1)}, f32[64,128]{1,0:T(8,128)S(1)}, u32[]{:S(2)}, u32[]{:S(2)}) collective-permute-start(f32[64,128]{1,0:T(8,128)S(1)} %get-tuple-element.38), channel_id=1, source_target_pairs={{0,4},{4,0},{8,12},{12,8},{1,5},{5,1},{9,13},{13,9},{2,6},{6,2},{1... | collective-permute-start | bytes 98312 | tf_op jit(solution)/shard_map/ppermute | solution.py:82
  (1 other events, 0.7 us)
where the time goes:
time: 167 us; the launch traced here: 166 us
  waiting for transfers between devices  74.3 us (44%)
  Pallas kernels  57.8 us (35%)
  starting transfers between devices  27.9 us (17%)
  local copies, waits for them, and re-layouts  4.37 us (3%)
    ppermute x9, waiting for transfers between devices, exchange(): lax.ppermute(block, axis, [(a, b) for a, b in pairs] + [(b, a) for a, b i...  39.9 us
    ppermute x2, waiting for transfers between devices, apply_shifted(): lax.ppermute(mine, 'vec', [(i, i ^ step) for i in range(lanes)])  25 us
    ppermute x9, starting transfers between devices, exchange(): lax.ppermute(block, axis, [(a, b) for a, b in pairs] + [(b, a) for a, b i...  12.8 us
    ppermute x9, starting transfers between devices, all_sum(): lax.ppermute(block, axis, [(i, i ^ mask) for i in range(size)])  11.8 us
    pallas_call x1, Pallas kernels, local(): call(third_body, [full, full, (width, 2 * width)], [SMEM] + [VMEM] * 5, [...  9.81 us
    pallas_call x2, Pallas kernels, apply_shifted(): call(join_body, [halfshape] * 2, [SMEM] * (3 + count) + [VMEM] * (count +...  8.2 us
    pallas_call x2, Pallas kernels, apply_shifted(): call(own_body, [full], [SMEM] * 3 + [VMEM] * 3, name='own')  7.96 us
    pallas_call x1, Pallas kernels, local(): call(second_body, [square, square, (width, 3 * width)], [VMEM] * 2, name=...  6.47 us
  transfers between devices with their start and end apart: 24, of which 15 were waited for; matrix products, arithmetic and copies ran while one was open for 0% of the time, Pallas kernels for 13%

commit v1 on v0

v1 whole, which is shorter than its diff:
```python
import math

import jax
import jax.numpy as jnp
from jax import lax
from jax.experimental import pallas as pl
from jax.experimental.pallas import tpu as pltpu
from jax.sharding import PartitionSpec as P

OWN_SLOTS = 20
HOPS = 3
CAP = 8
SHIFT = 1.65
BF16 = jnp.bfloat16
F32 = jnp.float32

VMEM = pl.BlockSpec(memory_space=pltpu.VMEM)
SMEM = pl.BlockSpec(memory_space=pltpu.SMEM)
ANY = pl.BlockSpec(memory_space=pl.ANY)


def contract(a, b, ta=False, tb=False, precision=None):
    dims = (((0 if ta else 1,), (1 if tb else 0,)), ((), ()))
    return lax.dot_general(a, b, dims, precision=precision, preferred_element_type=F32)


def dot(a, b, ta=False, tb=False):
    return contract(a, b, ta, tb, lax.Precision.HIGHEST)


def pieces(x, count):
    out = []
    for _ in range(count):
        out.append(x.astype(BF16))
        x = x - out[-1].astype(F32)
    return out


def tile_product(x, tile_ref, slot, transposed):
    x1, x2 = pieces(x, 2)
    m1, m2 = tile_ref[slot, 0], tile_ref[slot, 1]
    axis = 1 if transposed else 0
    left = jnp.concatenate([x1, x2, x1], axis=1)
    return contract(left, jnp.concatenate([m1, m1, m2], axis=axis), tb=transposed)


def wide_product(coef, blocks):
    c1, c2, c3 = pieces(coef, 3)
    z1, z2, z3 = pieces(jnp.concatenate(blocks, axis=1), 3)
    left = jnp.concatenate([c1, c1, c1, c2, c2, c3], axis=1)
    out = contract(left, jnp.concatenate([z1, z2, z3, z1, z2, z1], axis=0))
    width = blocks[0].shape[1]
    return [out[:, n * width : (n + 1) * width] for n in range(len(blocks))]


def gram_step(left, right):
    a = jnp.concatenate(pieces(jnp.concatenate(left, axis=1), 2), axis=0)
    b = jnp.concatenate(
        [p for group in right for p in pieces(jnp.concatenate(group, axis=1), 2)], axis=0
    )
    out = contract(a, b, tb=True)
    size = left[0].shape[0]
    out = out[:size] + out[size:]
    return jnp.concatenate(
        [
            out[:, 2 * g * size : (2 * g + 1) * size] + out[:, (2 * g + 1) * size : (2 * g + 2) * size]
            for g in range(len(right))
        ],
        axis=1,
    )


def call(body, outs, in_specs, scratch=(), name=None, aliases=None):
    shapes = [
        o if isinstance(o, jax.ShapeDtypeStruct) else jax.ShapeDtypeStruct(o, F32) for o in outs
    ]
    return pl.pallas_call(
        body,
        out_shape=shapes,
        in_specs=in_specs,
        out_specs=[VMEM] * len(outs),
        scratch_shapes=list(scratch),
        compiler_params=pltpu.CompilerParams(vmem_limit_bytes=40 << 20),
        input_output_aliases=aliases or {},
        name=name,
    )


def after(value, *tokens):
    return lax.optimization_barrier((value,) + tokens)[0]


def pairings(size):
    rounds = []
    for hop in range(1, HOPS + 1):
        for parity in range(2):
            pairs = [(i, i + hop) for i in range(size - hop) if (i // hop) % 2 == parity]
            if not pairs:
                continue
            used = {i for pair in pairs for i in pair}
            for entry in rounds:
                if not entry["used"] & used:
                    entry["used"] |= used
                    entry["pairs"] += pairs
                    entry["kinds"].append((hop, parity))
                    break
            else:
                rounds.append({"used": used, "pairs": pairs, "kinds": [(hop, parity)]})
    return rounds


def exchange(block, axis, pairs):
    return lax.ppermute(block, axis, [(a, b) for a, b in pairs] + [(b, a) for a, b in pairs])


def role_table(rounds, size):
    table = [[0] * size for _ in rounds]
    for p, entry in enumerate(rounds):
        for a, b in entry["pairs"]:
            table[p][a] = b - a
            table[p][b] = a - b
    return jnp.array(table, jnp.int32)


def all_sum(block, axis):
    size = lax.axis_size(axis)
    if size & (size - 1):
        return lax.psum(block, axis)
    step = 1
    while step < size:
        masks = [step] if step * 2 >= size else [step, 2 * step, 3 * step]
        got = [lax.ppermute(block, axis, [(i, i ^ mask) for i in range(size)]) for mask in masks]
        if len(got) == 1:
            block = block + got[0]
            step *= 2
        else:
            block = (block + got[0]) + (got[1] + got[2])
            step *= 4
    return block


def factor(gram):
    size = gram.shape[0]
    row_id = lax.broadcasted_iota(jnp.int32, (size, size), 0)
    col_id = lax.broadcasted_iota(jnp.int32, (size, size), 1)
    work = jnp.concatenate([gram, (row_id == col_id).astype(F32)], axis=1)
    blocks = [work[8 * b : 8 * b + 8] for b in range(size // 8)]
    sub = lax.broadcasted_iota(jnp.int32, (8, 2 * size), 0)
    for j in range(size):
        b, s = divmod(j, 8)
        row = blocks[b][s : s + 1]
        scaled = row / row[:, j : j + 1]
        scaled = jnp.broadcast_to(scaled, (8, 2 * size))
        for other in range(b, size // 8):
            col = jnp.broadcast_to(blocks[other][:, j : j + 1], (8, 2 * size))
            if other == b:
                col = jnp.where(sub > s, col, 0.0)
            blocks[other] = blocks[other] - col * scaled
    work = jnp.concatenate(blocks, axis=0)
    pivots = jnp.sum(jnp.where(row_id == col_id, work[:, :size], 0.0), axis=1, keepdims=True)
    work = work / jnp.sqrt(pivots)
    upper = jnp.where(col_id >= row_id, work[:, :size], 0.0)
    inverse = jnp.where(col_id <= row_id, work[:, size:], 0.0)
    return upper, inverse


def local(start_block, diagonal, hess_tiles, tile_rows, tile_cols, slot_counts):
    peers = lax.axis_size("res")
    lanes = lax.axis_size("vec")
    rows, width, length = start_block.shape
    slots = hess_tiles.shape[2]
    half = rows // 2
    part = width // 2
    rounds = pairings(peers)
    count = len(rounds)
    full = (rows, width, length)
    chunk = (rows, part, length)
    halfchunk = (half, part, length)
    packet = (CAP, part, length)
    square = (width, width)
    split_shape = jax.ShapeDtypeStruct((slots, 2, length, length), BF16)

    table = role_table(rounds, peers)
    place = jnp.concatenate(
        [lax.axis_index("vec").reshape(1), table[:, lax.axis_index("res")]]
    ).astype(jnp.int32)

    def own_sum(acc_refs, x_of, split_ref, rows_ref, cols_ref):
        for s in range(OWN_SLOTS):
            i, j = rows_ref[0, 0, s], cols_ref[0, 0, s]
            direct = tile_product(x_of(j), split_ref, s, True)
            mirror = tile_product(x_of(i), split_ref, s, False)
            for n, acc_ref in enumerate(acc_refs):
                acc_ref[i] += direct[n * part : (n + 1) * part]
                acc_ref[j] += mirror[n * part : (n + 1) * part]

    def prepare_body(place_ref, rows_ref, cols_ref, x_ref, diag_ref, tiles_ref, split_ref, a_ref, b_ref, raw_ref, sem):
        size = slots // 4
        copies = [
            pltpu.make_async_copy(
                tiles_ref.at[0, 0, pl.ds(n * size, size)], raw_ref.at[pl.ds(n * size, size)], sem.at[n]
            )
            for n in range(4)
        ]
        for c in copies:
            c.start()
        first = (place_ref[0] == 0).astype(F32)
        d = ((diag_ref[...] - SHIFT) * first)[:, None, :]
        a_ref[...] = x_ref[:, :part] * d
        b_ref[...] = x_ref[:, part:] * d
        for n in range(4):
            copies[n].wait()
            for s in range(n * size, (n + 1) * size):
                split_ref[s, 0], split_ref[s, 1] = pieces(raw_ref[s], 2)
        own_sum([a_ref, b_ref], lambda i: x_ref[i], split_ref, rows_ref, cols_ref)

    def own_body(place_ref, rows_ref, cols_ref, x_ref, diag_ref, split_ref, acc_ref):
        first = (place_ref[0] == 0).astype(F32)
        acc_ref[...] = x_ref[...] * ((diag_ref[...] - SHIFT) * first)[:, None, :]
        own_sum([acc_ref], lambda i: x_ref[i], split_ref, rows_ref, cols_ref)

    def pack(place_ref, rows_ref, counts_ref, asked_refs, x_ref, split_ref, outs):
        for p in range(count):
            role = place_ref[1 + p]

            def put(c, value, p=p):
                for n, ref in enumerate(outs[p]):
                    ref[c] = value[n * part : (n + 1) * part]

            @pl.when(role > 0)
            def _():
                base = OWN_SLOTS + (role - 1) * CAP
                for c in range(CAP):
                    term = tile_product(x_ref[rows_ref[0, 0, base + c]], split_ref, base + c, False)
                    put(c, jnp.where(c < counts_ref[0, 0, role - 1], term, 0.0))

            @pl.when(role < 0)
            def _():
                base = OWN_SLOTS + (-role - 1) * CAP
                for c in range(CAP):
                    put(c, x_ref[asked_refs[p][0, 0, base + c]])

    def send_body(place_ref, rows_ref, counts_ref, *refs):
        asked_refs, (x_ref, split_ref), outs = refs[:count], refs[count : count + 2], refs[count + 2 :]
        pack(
            place_ref, rows_ref, counts_ref, asked_refs, x_ref, split_ref,
            [(outs[p], outs[count + p]) for p in range(count)],
        )

    def settle(place_ref, mine_ref, other_ref, y_ref):
        core = place_ref[0] % 2
        y_ref[pl.ds(core * half, half)] = mine_ref[...]
        y_ref[pl.ds((1 - core) * half, half)] = other_ref[...]

    def resend_body(place_ref, rows_ref, counts_ref, *refs):
        asked_refs = refs[:count]
        mine_ref, other_ref, split_ref, y_ref = refs[count : count + 4]
        outs = refs[count + 4 :]
        settle(place_ref, mine_ref, other_ref, y_ref)
        pack(
            place_ref, rows_ref, counts_ref, asked_refs, y_ref, split_ref,
            [(outs[p],) for p in range(count)],
        )

    def join_body(place_ref, rows_ref, counts_ref, *refs):
        asked_refs, got_refs = refs[:count], refs[count : 2 * count]
        split_ref, part_ref, keep_ref, give_ref, acc_ref = refs[2 * count :]
        acc_ref[...] = part_ref[...]
        for p in range(count):
            role = place_ref[1 + p]

            @pl.when(role > 0)
            def _():
                base = OWN_SLOTS + (role - 1) * CAP
                for c in range(CAP):
                    term = tile_product(got_refs[p][c], split_ref, base + c, True)
                    acc_ref[rows_ref[0, 0, base + c]] += jnp.where(
                        c < counts_ref[0, 0, role - 1], term, 0.0
                    )

            @pl.when(role < 0)
            def _():
                base = OWN_SLOTS + (-role - 1) * CAP
                for c in range(CAP):
                    acc_ref[asked_refs[p][0, 0, base + c]] += got_refs[p][c]

        core = place_ref[0] % 2
        keep_ref[...] = acc_ref[pl.ds(core * half, half)]
        give_ref[...] = acc_ref[pl.ds((1 - core) * half, half)]

    def gram_body(x_ref, out_ref):
        total = jnp.zeros(square, F32)
        for n in range(0, rows, 2):
            pair = [x_ref[n], x_ref[n + 1]]
            total += gram_step(pair, [pair])
        out_ref[...] = total

    def cross_body(x_ref, a_ref, b_ref, out_ref):
        total = jnp.zeros((width, 2 * width), F32)
        for n in range(0, rows, 2):
            y = [jnp.concatenate([a_ref[m], b_ref[m]], axis=0) for m in (n, n + 1)]
            total += gram_step(y, [[x_ref[n], x_ref[n + 1]], y])
        out_ref[...] = total

    def first_body(gram_ref, inverse_ref):
        _, inverse_ref[...] = factor(gram_ref[...])

    def identity():
        eye = lax.broadcasted_iota(jnp.int32, square, 0) == lax.broadcasted_iota(jnp.int32, square, 1)
        return eye.astype(F32)

    def second_body(gram_ref, inverse_ref, cross_ref, lower_ref, coef_ref, gain_ref):
        start_inv = inverse_ref[...]
        cross = dot(dot(start_inv, gram_ref[:, :width]), start_inv, tb=True)
        applied = dot(dot(start_inv, gram_ref[:, width:]), start_inv, tb=True)
        upper, inverse = factor(applied - dot(cross, cross, tb=True))
        lower = upper.T
        cross_ref[...] = cross + SHIFT * identity()
        lower_ref[...] = lower
        gain = dot(inverse, start_inv)
        back = -dot(dot(inverse, cross), start_inv)
        gain_ref[...] = gain
        coef_ref[:width, :width] = -dot(lower, start_inv)
        coef_ref[:width, width:] = back
        coef_ref[width:, :width] = back
        coef_ref[width:, width:] = gain

    def blend_body(x_ref, a_ref, b_ref, coef_ref, w_ref, q_ref, out_ref):
        total = jnp.zeros(square, F32)
        for n in range(0, rows, 2):
            qs = []
            stacks = [
                jnp.concatenate([x_ref[m], a_ref[m], b_ref[m]], axis=0) for m in (n, n + 1)
            ]
            for m, both in zip((n, n + 1), wide_product(coef_ref[...], stacks)):
                w_ref[m] = both[:width]
                q_ref[m] = both[width:]
                qs.append(both[width:])
            total += gram_step(qs, [qs])
        out_ref[...] = total

    def third_body(place_ref, *refs):
        mine_refs, other_refs = refs[0:2], refs[2:4]
        prior_ref, q_ref, gain_ref, norm_ref, w_ref, out_ref = refs[4:10]
        z_refs = refs[10:12]
        for n in range(2):
            settle(place_ref, mine_refs[n], other_refs[n], z_refs[n])
        total = jnp.zeros((width, 2 * width), F32)
        for n in range(0, rows, 2):
            zs = [jnp.concatenate([z_refs[0][m], z_refs[1][m]], axis=0) for m in (n, n + 1)]
            ws = []
            for m, w in zip((n, n + 1), wide_product(gain_ref[...], zs)):
                w = w + prior_ref[m]
                w_ref[m] = w
                ws.append(w)
            total += gram_step(ws, [[q_ref[n], q_ref[n + 1]], ws])
        out_ref[:, : 2 * width] = total
        out_ref[:, 2 * width : 3 * width] = norm_ref[...]
        out_ref[:, 3 * width :] = jnp.zeros(square, F32)

    def fourth_body(gram_ref, cross_ref, lower_ref, coef_ref):
        cross = gram_ref[:, :width]
        norm = gram_ref[:, 2 * width : 3 * width]
        taken = cross + SHIFT * (norm - identity())
        mixed = dot(taken, cross, tb=True)
        squared = gram_ref[:, width : 2 * width] - mixed - mixed.T + dot(dot(taken, norm), taken, tb=True)
        upper, inverse = factor(squared)
        cross_ref[...] = taken + SHIFT * identity()
        lower_ref[...] = upper.T
        scale = math.sqrt(rows * length * peers)
        coef_ref[:, :width] = inverse * scale
        coef_ref[:, width:] = -dot(inverse, taken) * scale

    def last_body(w_ref, q_ref, coef_ref, a1_ref, l1_ref, a2_ref, l2_ref, out_ref, pack_ref):
        for n, ref in enumerate((a1_ref, l1_ref, a2_ref, l2_ref)):
            pack_ref[n] = ref[...]
        for n in range(0, rows, 2):
            stacks = [jnp.concatenate([w_ref[m], q_ref[m]], axis=0) for m in (n, n + 1)]
            for m, out in zip((n, n + 1), wide_product(coef_ref[...], stacks)):
                out_ref[m] = out

    swap = [(i, i ^ 1) for i in range(lanes)]

    def spread(sent):
        return [exchange(s, "res", entry["pairs"]) for s, entry in zip(sent, rounds)]

    def join(got, prior, token):
        return call(
            join_body,
            [halfchunk] * 2,
            [SMEM] * (3 + count) + [VMEM] * (count + 2),
            [pltpu.VMEM(chunk, F32)],
            name="join",
        )(place, tile_rows, slot_counts, *asked, *got, split, after(prior, token))

    def vec_sum(keep, give, token=None):
        mine = keep + lax.ppermute(give, "vec", swap)
        step = 2
        while step < lanes:
            got = lax.ppermute(mine, "vec", [(i, i ^ step) for i in range(lanes)])
            if token is not None:
                got = after(got, token)
            mine = mine + got
            step *= 2
        return mine, lax.ppermute(mine, "vec", swap)

    def resend(mine, other, token):
        y, *sent = call(
            resend_body, [chunk] + [packet] * count, [SMEM] * (3 + count) + [VMEM] * 3, name="resend"
        )(place, tile_rows, slot_counts, *asked, mine, after(other, token), split)
        return y, sent

    def own(y, token):
        (acc,) = call(own_body, [chunk], [SMEM] * 3 + [VMEM] * 3, name="own")(
            place, tile_rows, tile_cols, after(y, token), diagonal, split
        )
        return acc

    asked = [exchange(tile_cols, "res", entry["pairs"]) for entry in rounds]
    split, prior_a, prior_b = call(
        prepare_body,
        [split_shape, chunk, chunk],
        [SMEM] * 3 + [VMEM] * 2 + [ANY],
        [pltpu.VMEM((slots, length, length), F32), pltpu.SemaphoreType.DMA((4,))],
        name="prepare",
    )(place, tile_rows, tile_cols, start_block, diagonal, hess_tiles)
    sent = call(
        send_body, [packet] * (2 * count), [SMEM] * (3 + count) + [VMEM] * 2, name="send"
    )(place, tile_rows, slot_counts, *asked, start_block, split)
    got_a = spread(sent[:count])
    got_b = spread(sent[count:])
    (start_gram,) = call(gram_body, [square], [VMEM], name="gram")(after(start_block, sent[0]))
    start_total = all_sum(start_gram, "res")
    keep, give = join(got_a, prior_a, start_gram)
    (start_inv,) = call(first_body, [square], [VMEM], name="first")(after(start_total, keep))
    mine, other = vec_sum(keep, give, start_inv)
    y_a, sent = resend(mine, other, start_inv)
    got_a = spread(sent)
    keep, give = join(got_b, prior_b, y_a)
    prior_a = own(y_a, keep)
    mine, other = vec_sum(keep, give, prior_a)
    y_b, sent = resend(mine, other, prior_a)
    got_b = spread(sent)
    (cross_gram,) = call(cross_body, [(width, 2 * width)], [VMEM] * 3, name="cross")(
        start_block, y_a, y_b
    )
    cross_total = all_sum(cross_gram, "res")
    prior_b = own(y_b, cross_gram)
    cross1, lower1, coef, gain = call(
        second_body, [square, square, (2 * width, 2 * width), square], [VMEM] * 2, name="second"
    )(after(cross_total, prior_b), start_inv)
    w_prior, q, norm = call(blend_body, [full, full, square], [VMEM] * 4, name="blend")(
        start_block, y_a, y_b, coef
    )
    keep_a, give_a = join(got_a, prior_a, norm)
    mine_a, other_a = vec_sum(keep_a, give_a)
    keep_b, give_b = join(got_b, prior_b, keep_a)
    mine_b, other_b = vec_sum(keep_b, give_b)
    w, gram = call(
        third_body,
        [full, (width, 4 * width)],
        [SMEM] + [VMEM] * 8,
        [pltpu.VMEM(chunk, F32)] * 2,
        name="third",
    )(place, mine_a, mine_b, other_a, other_b, w_prior, q, gain, norm)
    gram = all_sum(gram, "res")
    cross2, lower2, coef = call(
        fourth_body, [square, square, (width, 2 * width)], [VMEM], name="fourth"
    )(gram)
    return call(last_body, [full, (4, width, width)], [VMEM] * 7, name="last")(
        w, q, coef, cross1, lower1, cross2, lower2
    )


def solution(mesh):
    in_specs = (
        P(("conf", "res"), None, None),
        P(("conf", "res"), None),
        P(("conf", "res"), "vec", None, None, None),
        P(("conf", "res"), "vec", None),
        P(("conf", "res"), "vec", None),
        P(("conf", "res"), "vec", None),
    )
    out_specs = (P(("conf", "res"), None, None), P("conf", None, None))
    return jax.shard_map(local, mesh=mesh, in_specs=in_specs, out_specs=out_specs, check_vma=False)
```

time: 167 us -> 147 us (0.88)
  waiting for transfers between devices: 74.3 us -> 54.3 us
  Pallas kernels: 57.8 us -> 48 us
  starting transfers between devices: 27.9 us -> 37.1 us
    ppermute x9 -> x15, waiting for transfers between devices: 39.9 us -> 23.1 us  [exchange(): lax.ppermute(block, axis, [(a, b) for a, b in pairs] + [(b, a) for a, b i...]
    pallas_call x12 -> x17, Pallas kernels: 51.8 us -> 41.8 us  [the longest x4 7.53 us: join(): call(join_body, [halfchunk] * 2, [SMEM] * (3 + count) + [VMEM] * (count +...]
    ppermute x9 -> x15, starting transfers between devices: 12.8 us -> 19.7 us  [exchange(): lax.ppermute(block, axis, [(a, b) for a, b in pairs] + [(b, a) for a, b i...]
    ppermute x6 -> x12, waiting for transfers between devices: 30.6 us -> 25 us  [the longest x4 18.1 us: vec_sum(): got = lax.ppermute(mine, 'vec', [(i, i ^ step) for i in range(lanes)])]
    ppermute x9, waiting for transfers between devices: 3.78 us -> 6.21 us  [all_sum(): lax.ppermute(block, axis, [(i, i ^ mask) for i in range(size)])]
    unnamed x18 -> x20, local copies, waits for them, and re-layouts: 4.37 us -> 5.09 us
    ppermute x6 -> x12, starting transfers between devices: 3.39 us -> 4.02 us  [the longest x4 3.45 us: vec_sum(): got = lax.ppermute(mine, 'vec', [(i, i ^ step) for i in range(lanes)])]
  transfers between devices with their start and end apart: 24 -> 36, of which waited for: 15 -> 19; matrix products, arithmetic and copies ran while one was open for 0% -> 1% of each run, Pallas kernels for 13% -> 22%
where the time goes in v1:
time: 147 us
  waiting for transfers between devices  54.3 us (37%)
  Pallas kernels  48 us (33%)
  starting transfers between devices  37.1 us (25%)
  local copies, waits for them, and re-layouts  5.78 us (4%)
    ppermute x15, waiting for transfers between devices, exchange(): lax.ppermute(block, axis, [(a, b) for a, b in pairs] + [(b, a) for a, b i...  23.1 us
    ppermute x15, starting transfers between devices, exchange(): lax.ppermute(block, axis, [(a, b) for a, b in pairs] + [(b, a) for a, b i...  19.7 us
    ppermute x4, waiting for transfers between devices, vec_sum(): got = lax.ppermute(mine, 'vec', [(i, i ^ step) for i in range(lanes)])  18.1 us
    ppermute x9, starting transfers between devices, all_sum(): lax.ppermute(block, axis, [(i, i ^ mask) for i in range(size)])  13.3 us
    pallas_call x4, Pallas kernels, join(): call(join_body, [halfchunk] * 2, [SMEM] * (3 + count) + [VMEM] * (count +...  7.53 us
    pallas_call x1, Pallas kernels, local(): call(second_body, [square, square, (2 * width, 2 * width), square], [VMEM...  6.48 us
    pallas_call x1, Pallas kernels, local(): call(fourth_body, [square, square, (width, 2 * width)], [VMEM], name='fou...  6.25 us
    ppermute x9, waiting for transfers between devices, all_sum(): lax.ppermute(block, axis, [(i, i ^ mask) for i in range(size)])  6.21 us
  transfers between devices with their start and end apart: 36, of which 19 were waited for; matrix products, arithmetic and copies ran while one was open for 1% of the time, Pallas kernels for 22%

profile of v1, /device:TPU:0, one launch (start us, length us, event | category | flops | bytes accessed | tf_op | source)
XLA Modules:
  0.0 146.6 jit_solution(8556867404010488077)
XLA Ops:
  0.6 4.1 %collective-permute-start.2 = (s32[1,1,44]{2,1,0:T(1,128)}, s32[1,1,44]{2,1,0:T(1,128)S(1)}, u32[]{:S(2)}, u32[]{:S(2)}) collective-permute-start(s32[1,1,44]{2,1,0:T(1,128)} %cols_ref.5), channel_id=1, source_target_pairs={{0,8},{4,12},{8,0},{12,4},{1,9},{5,13},{9,1},{13,5},{2,10},{6,14},... | collective-permute-start | bytes 536 | tf_op jit(solution)/shard_map/ppermute | solution.py:113
  8.3 1.8 %copy-done.2 = f32[1,1,44,128,128]{4,3,2,1,0:T(8,128)S(1)} copy-done((f32[1,1,44,128,128]{4,3,2,1,0:T(8,128)S(1)}, f32[1,1,44,128,128]{4,3,2,1,0:T(8,128)}, u32[]{:S(2)}) %copy-start.2) | copy-done | bytes 2883608
  12.2 3.4 %prepare.1 = (bf16[44,2,128,128]{3,2,1,0:T(8,128)(2,1)S(1)}, f32[32,32,128]{2,1,0:T(8,128)S(1)}, f32[32,32,128]{2,1,0:T(8,128)S(1)}) custom-call(s32[4]{0:T(128)S(1)} %pad_add_fusion.place_ref, s32[1,1,44]{2,1,0:T(1,128)S(1)} %copy-done.5, s32[1,1,44]{2,1,0:T(1,128)S(1)} %copy-done.8, f32[32,64,128]{2,1,0:T(8,128)S(1)} %copy-done, f32[32,128]{1,0:T(8,128)S(1)} %copy-done.3, ...), custom_call_target="tpu_custom_call" | custom-call | tf_op jit(solution)/shard_map/prepare/pallas_call | solution.py:420
  17.1 2.2 %collective-permute-start.4 = (f32[8,32,128]{2,1,0:T(8,128)S(1)}, f32[8,32,128]{2,1,0:T(8,128)S(1)}, u32[]{:S(2)}, u32[]{:S(2)}) collective-permute-start(f32[8,32,128]{2,1,0:T(8,128)S(1)} %get-tuple-element.54), channel_id=1, source_target_pairs={{4,8},{0,12},{8,4},{12,0},{5,9},{1,13},{9,5},{13,1},{6,10},{2,14},... | collective-permute-start | bytes 393224 | tf_op jit(solution)/shard_map/ppermute | solution.py:113
  22.1 3.3 %collective-permute-done.4.refs_4_ = f32[8,32,128]{2,1,0:T(8,128)S(1)} collective-permute-done((f32[8,32,128]{2,1,0:T(8,128)S(1)}, f32[8,32,128]{2,1,0:T(8,128)S(1)}, u32[]{:S(2)}, u32[]{:S(2)}) %collective-permute-start.4) | collective-permute-done | bytes 131104 | tf_op jit(solution)/shard_map/ppermute | solution.py:113
  25.4 5.6 %collective-permute-done.5.refs_5_ = f32[8,32,128]{2,1,0:T(8,128)S(1)} collective-permute-done((f32[8,32,128]{2,1,0:T(8,128)S(1)}, f32[8,32,128]{2,1,0:T(8,128)S(1)}, u32[]{:S(2)}, u32[]{:S(2)}) %collective-permute-start.5) | collective-permute-done | bytes 131104 | tf_op jit(solution)/shard_map/ppermute | solution.py:113
  31.0 1.8 %join.4 = (f32[16,32,128]{2,1,0:T(8,128)S(1)}, f32[16,32,128]{2,1,0:T(8,128)S(1)}) custom-call(s32[4]{0:T(128)S(1)} %pad_add_fusion.place_ref, s32[1,1,44]{2,1,0:T(1,128)S(1)} %copy-done.5, s32[1,1,3]{2,1,0:T(1,128)S(1)} %copy-done.7, s32[1,1,44]{2,1,0:T(1,128)S(1)} %collective-permute-done.refs_0_, s32[1,1,44]{2,1,0:T(1,128)S(1)} %collective-permute-done.1.refs_1_, ...), custom_call_target="tpu_custom_call" | custom-call | tf_op jit(solution)/shard_map/join/pallas_call | solution.py:388
  37.2 3.2 %collective-permute-start.8 = (f32[64,64]{1,0:T(8,128)S(1)}, f32[64,64]{1,0:T(8,128)S(1)}, u32[]{:S(2)}, u32[]{:S(2)}) collective-permute-start(f32[64,64]{1,0:T(8,128)S(1)} %gram.1), channel_id=1, source_target_pairs={{0,4},{4,0},{8,12},{12,8},{1,5},{5,1},{9,13},{13,9},{2,6},{6,2},{1... | collective-permute-start | bytes 49160 | tf_op jit(solution)/shard_map/ppermute | solution.py:132
  40.4 1.6 %collective-permute-done.10 = f32[64,64]{1,0:T(8,128)S(1)} collective-permute-done((f32[64,64]{1,0:T(8,128)S(1)}, f32[64,64]{1,0:T(8,128)S(1)}, u32[]{:S(2)}, u32[]{:S(2)}) %collective-permute-start.10) | collective-permute-done | bytes 16416 | tf_op jit(solution)/shard_map/ppermute | solution.py:132
  42.6 5.5 %first.1.inverse_ref = f32[64,64]{1,0:T(8,128)S(1)} custom-call(f32[64,64]{1,0:T(8,128)S(1)} %add_add_fusion.2.gram_ref), custom_call_target="tpu_custom_call" | custom-call | tf_op jit(solution)/shard_map/first/pallas_call | solution.py:435
  48.2 1.8 %collective-permute-start.15 = (f32[8,32,128]{2,1,0:T(8,128)S(1)}, f32[8,32,128]{2,1,0:T(8,128)S(1)}, u32[]{:S(2)}, u32[]{:S(2)}) collective-permute-start(f32[8,32,128]{2,1,0:T(8,128)S(1)} %get-tuple-element.68), channel_id=1, source_target_pairs={{0,4},{8,12},{4,0},{12,8},{1,5},{9,13},{5,1},{13,9},{2,6},{10,14},... | collective-permute-start | bytes 393224 | tf_op jit(solution)/shard_map/ppermute | solution.py:113
  54.2 4.2 %collective-permute-done.16.refs_4_ = f32[8,32,128]{2,1,0:T(8,128)S(1)} collective-permute-done((f32[8,32,128]{2,1,0:T(8,128)S(1)}, f32[8,32,128]{2,1,0:T(8,128)S(1)}, u32[]{:S(2)}, u32[]{:S(2)}) %collective-permute-start.16) | collective-permute-done | bytes 131104 | tf_op jit(solution)/shard_map/ppermute | solution.py:113
  58.3 5.5 %collective-permute-done.17.refs_5_ = f32[8,32,128]{2,1,0:T(8,128)S(1)} collective-permute-done((f32[8,32,128]{2,1,0:T(8,128)S(1)}, f32[8,32,128]{2,1,0:T(8,128)S(1)}, u32[]{:S(2)}, u32[]{:S(2)}) %collective-permute-start.17) | collective-permute-done | bytes 131104 | tf_op jit(solution)/shard_map/ppermute | solution.py:113
  63.8 1.8 %join.5 = (f32[16,32,128]{2,1,0:T(8,128)S(1)}, f32[16,32,128]{2,1,0:T(8,128)S(1)}) custom-call(s32[4]{0:T(128)S(1)} %pad_add_fusion.place_ref, s32[1,1,44]{2,1,0:T(1,128)S(1)} %copy-done.6, s32[1,1,3]{2,1,0:T(1,128)S(1)} %copy-done.7, s32[1,1,44]{2,1,0:T(1,128)S(1)} %collective-permute-done.refs_0_, s32[1,1,44]{2,1,0:T(1,128)S(1)} %collective-permute-done.1.refs_1_, ...), custom_call_target="tpu_custom_call" | custom-call | tf_op jit(solution)/shard_map/join/pallas_call | solution.py:388
  67.9 1.7 %own.2.refs_7_ = f32[32,32,128]{2,1,0:T(8,128)S(1)} custom-call(s32[4]{0:T(128)S(1)} %pad_add_fusion.place_ref, s32[1,1,44]{2,1,0:T(1,128)S(1)} %copy-done.6, s32[1,1,44]{2,1,0:T(1,128)S(1)} %copy-done.9, f32[32,32,128]{2,1,0:T(8,128)S(1)} %get-tuple-element.74.x_ref.a_ref, f32[32,128]{1,0:T(8,128)S(1)} %copy-done.4, ...), custom_call_target="tpu_custom_call" | custom-call | tf_op jit(solution)/shard_map/own/pallas_call | solution.py:414
  69.6 6.1 %collective-permute-done.19 = f32[16,32,128]{2,1,0:T(8,128)S(1)} collective-permute-done((f32[16,32,128]{2,1,0:T(8,128)S(1)}, f32[16,32,128]{2,1,0:T(8,128)S(1)}, u32[]{:S(2)}, u32[]{:S(2)}) %collective-permute-start.19) | collective-permute-done | bytes 262176 | tf_op jit(solution)/shard_map/ppermute | solution.py:400
  81.8 2.6 %collective-permute-start.21 = (f32[64,128]{1,0:T(8,128)S(1)}, f32[64,128]{1,0:T(8,128)S(1)}, u32[]{:S(2)}, u32[]{:S(2)}) collective-permute-start(f32[64,128]{1,0:T(8,128)S(1)} %cross.1), channel_id=1, source_target_pairs={{0,4},{4,0},{8,12},{12,8},{1,5},{5,1},{9,13},{13,9},{2,6},{6,2},{1... | collective-permute-start | bytes 98312 | tf_op jit(solution)/shard_map/ppermute | solution.py:132
  84.7 1.7 %own.3.refs_7_ = f32[32,32,128]{2,1,0:T(8,128)S(1)} custom-call(s32[4]{0:T(128)S(1)} %pad_add_fusion.place_ref, s32[1,1,44]{2,1,0:T(1,128)S(1)} %copy-done.6, s32[1,1,44]{2,1,0:T(1,128)S(1)} %copy-done.9, f32[32,32,128]{2,1,0:T(8,128)S(1)} %get-tuple-element.79.b_ref.x_ref, f32[32,128]{1,0:T(8,128)S(1)} %copy-done.4, ...), custom_call_target="tpu_custom_call" | custom-call | tf_op jit(solution)/shard_map/own/pallas_call | solution.py:414
  87.7 2.9 %collective-permute-start.26 = (f32[8,32,128]{2,1,0:T(8,128)S(1)}, f32[8,32,128]{2,1,0:T(8,128)S(1)}, u32[]{:S(2)}, u32[]{:S(2)}) collective-permute-start(f32[8,32,128]{2,1,0:T(8,128)S(1)} %get-tuple-element.86), channel_id=1, source_target_pairs={{0,4},{8,12},{4,0},{12,8},{1,5},{9,13},{5,1},{13,9},{2,6},{10,14},... | collective-permute-start | bytes 393224 | tf_op jit(solution)/shard_map/ppermute | solution.py:113
  92.1 6.5 %second.1 = (f32[64,64]{1,0:T(8,128)S(1)}, f32[64,64]{1,0:T(8,128)S(1)}, f32[128,128]{1,0:T(8,128)S(1)}, f32[64,64]{1,0:T(8,128)S(1)}) custom-call(f32[64,128]{1,0:T(8,128)S(1)} %add_add_fusion.1.gram_ref, f32[64,64]{1,0:T(8,128)S(1)} %first.1.inverse_ref), custom_call_target="tpu_custom_call" | custom-call | tf_op jit(solution)/shard_map/second/pallas_call | solution.py:449
  98.6 4.6 %blend.1 = (f32[32,64,128]{2,1,0:T(8,128)S(1)}, f32[32,64,128]{2,1,0:T(8,128)S(1)}, f32[64,64]{1,0:T(8,128)S(1)}) custom-call(f32[32,64,128]{2,1,0:T(8,128)S(1)} %copy-done.1, f32[32,32,128]{2,1,0:T(8,128)S(1)} %get-tuple-element.74.x_ref.a_ref, f32[32,32,128]{2,1,0:T(8,128)S(1)} %get-tuple-element.79.b_ref.x_ref, f32[128,128]{1,0:T(8,128)S(1)} %get-tuple-element.81.coef_ref), custom_call_target="tpu_custom_call" | custom-call | tf_op jit(solution)/shard_map/blend/pallas_call | solution.py:452
  104.0 1.8 %join.6 = (f32[16,32,128]{2,1,0:T(8,128)S(1)}, f32[16,32,128]{2,1,0:T(8,128)S(1)}) custom-call(s32[4]{0:T(128)S(1)} %pad_add_fusion.place_ref, s32[1,1,44]{2,1,0:T(1,128)S(1)} %copy-done.6, s32[1,1,3]{2,1,0:T(1,128)S(1)} %copy-done.7, s32[1,1,44]{2,1,0:T(1,128)S(1)} %collective-permute-done.refs_0_, s32[1,1,44]{2,1,0:T(1,128)S(1)} %collective-permute-done.1.refs_1_, ...), custom_call_target="tpu_custom_call" | custom-call | tf_op jit(solution)/shard_map/join/pallas_call | solution.py:388
  105.9 2.8 %collective-permute-done.28.refs_5_ = f32[8,32,128]{2,1,0:T(8,128)S(1)} collective-permute-done((f32[8,32,128]{2,1,0:T(8,128)S(1)}, f32[8,32,128]{2,1,0:T(8,128)S(1)}, u32[]{:S(2)}, u32[]{:S(2)}) %collective-permute-start.28) | collective-permute-done | bytes 131104 | tf_op jit(solution)/shard_map/ppermute | solution.py:113
  108.7 2.0 %join.7 = (f32[16,32,128]{2,1,0:T(8,128)S(1)}, f32[16,32,128]{2,1,0:T(8,128)S(1)}) custom-call(s32[4]{0:T(128)S(1)} %pad_add_fusion.place_ref, s32[1,1,44]{2,1,0:T(1,128)S(1)} %copy-done.6, s32[1,1,3]{2,1,0:T(1,128)S(1)} %copy-done.7, s32[1,1,44]{2,1,0:T(1,128)S(1)} %collective-permute-done.refs_0_, s32[1,1,44]{2,1,0:T(1,128)S(1)} %collective-permute-done.1.refs_1_, ...), custom_call_target="tpu_custom_call" | custom-call | tf_op jit(solution)/shard_map/join/pallas_call | solution.py:388
  113.1 7.0 %collective-permute-done.25 = f32[16,32,128]{2,1,0:T(8,128)S(1)} collective-permute-done((f32[16,32,128]{2,1,0:T(8,128)S(1)}, f32[16,32,128]{2,1,0:T(8,128)S(1)}, u32[]{:S(2)}, u32[]{:S(2)}) %collective-permute-start.25) | collective-permute-done | bytes 262176 | tf_op jit(solution)/shard_map/ppermute | solution.py:400
  120.2 5.1 %collective-permute-done.30 = f32[16,32,128]{2,1,0:T(8,128)S(1)} collective-permute-done((f32[16,32,128]{2,1,0:T(8,128)S(1)}, f32[16,32,128]{2,1,0:T(8,128)S(1)}, u32[]{:S(2)}, u32[]{:S(2)}) %collective-permute-start.30) | collective-permute-done | bytes 262176 | tf_op jit(solution)/shard_map/ppermute | solution.py:400
  126.9 2.5 %third.1 = (f32[32,64,128]{2,1,0:T(8,128)S(1)}, f32[64,256]{1,0:T(8,128)S(1)}) custom-call(s32[4]{0:T(128)S(1)} %pad_add_fusion.place_ref, f32[16,32,128]{2,1,0:T(8,128)S(1)} %add.66.refs_0_, f32[16,32,128]{2,1,0:T(8,128)S(1)} %add.68.refs_1_, f32[16,32,128]{2,1,0:T(8,128)S(1)} %collective-permute-done.31.refs_2_, ...), custom_call_target="tpu_custom_call" | custom-call | tf_op jit(solution)/shard_map/third/pallas_call | solution.py:459
  130.5 3.5 %collective-permute-start.33 = (f32[64,256]{1,0:T(8,128)S(1)}, f32[64,256]{1,0:T(8,128)S(1)}, u32[]{:S(2)}, u32[]{:S(2)}) collective-permute-start(f32[64,256]{1,0:T(8,128)S(1)} %get-tuple-element.96), channel_id=1, source_target_pairs={{0,4},{4,0},{8,12},{12,8},{1,5},{5,1},{9,13},{13,9},{2,6},{6,2},{1... | collective-permute-start | bytes 196616 | tf_op jit(solution)/shard_map/ppermute | solution.py:132
  134.0 2.4 %collective-permute-done.35 = f32[64,256]{1,0:T(8,128)S(1)} collective-permute-done((f32[64,256]{1,0:T(8,128)S(1)}, f32[64,256]{1,0:T(8,128)S(1)}, u32[]{:S(2)}, u32[]{:S(2)}) %collective-permute-start.35) | collective-permute-done | bytes 65568 | tf_op jit(solution)/shard_map/ppermute | solution.py:132
  136.4 1.7 %collective-permute-done.34 = f32[64,256]{1,0:T(8,128)S(1)} collective-permute-done((f32[64,256]{1,0:T(8,128)S(1)}, f32[64,256]{1,0:T(8,128)S(1)}, u32[]{:S(2)}, u32[]{:S(2)}) %collective-permute-start.34) | collective-permute-done | bytes 65568 | tf_op jit(solution)/shard_map/ppermute | solution.py:132
  138.0 6.3 %fourth.1 = (f32[64,64]{1,0:T(8,128)S(1)}, f32[64,64]{1,0:T(8,128)S(1)}, f32[64,128]{1,0:T(8,128)S(1)}) custom-call(f32[64,256]{1,0:T(8,128)S(1)} %add_add_fusion.gram_ref), custom_call_target="tpu_custom_call" | custom-call | tf_op jit(solution)/shard_map/fourth/pallas_call | solution.py:467
  144.3 2.3 %last.1 = (f32[32,64,128]{2,1,0:T(8,128)}, f32[4,64,64]{2,1,0:T(8,128)}) custom-call(f32[32,64,128]{2,1,0:T(8,128)S(1)} %get-tuple-element.95.w_ref, f32[32,64,128]{2,1,0:T(8,128)S(1)} %get-tuple-element.93.refs_5_.q_ref, f32[64,128]{1,0:T(8,128)S(1)} %get-tuple-element.97.coef_ref, f32[64,64]{1,0:T(8,128)S(1)} %get-tuple-element.98.a1_ref, ...), custom_call_target="tpu_custom_call" | custom-call | tf_op jit(solution)/shard_map/last/pallas_call | solution.py:470
  (91 shorter events, 36.1 us)
Async XLA Ops:
  0.6 15.0 %collective-permute-start.2 = (s32[1,1,44]{2,1,0:T(1,128)}, s32[1,1,44]{2,1,0:T(1,128)S(1)}, u32[]{:S(2)}, u32[]{:S(2)}) collective-permute-start(s32[1,1,44]{2,1,0:T(1,128)} %cols_ref.5), channel_id=1, source_target_pairs={{0,8},{4,12},{8,0},{12,4},{1,9},{5,13},{9,1},{13,5},{2,10},{6,14},... | collective-permute-start | bytes 536 | tf_op jit(solution)/shard_map/ppermute | solution.py:113
  4.7 10.9 %collective-permute-start.1 = (s32[1,1,44]{2,1,0:T(1,128)}, s32[1,1,44]{2,1,0:T(1,128)S(1)}, u32[]{:S(2)}, u32[]{:S(2)}) collective-permute-start(s32[1,1,44]{2,1,0:T(1,128)} %cols_ref.5), channel_id=1, source_target_pairs={{4,8},{0,12},{8,4},{12,0},{5,9},{1,13},{9,5},{13,1},{6,10},{2,14},... | collective-permute-start | bytes 536 | tf_op jit(solution)/shard_map/ppermute | solution.py:113
  6.1 9.6 %collective-permute-start = (s32[1,1,44]{2,1,0:T(1,128)}, s32[1,1,44]{2,1,0:T(1,128)S(1)}, u32[]{:S(2)}, u32[]{:S(2)}) collective-permute-start(s32[1,1,44]{2,1,0:T(1,128)} %cols_ref.5), channel_id=1, source_target_pairs={{0,4},{8,12},{4,0},{12,8},{1,5},{9,13},{5,1},{13,9},{2,6},{10,14},... | collective-permute-start | bytes 536 | tf_op jit(solution)/shard_map/ppermute | solution.py:113
  17.1 8.3 %collective-permute-start.4 = (f32[8,32,128]{2,1,0:T(8,128)S(1)}, f32[8,32,128]{2,1,0:T(8,128)S(1)}, u32[]{:S(2)}, u32[]{:S(2)}) collective-permute-start(f32[8,32,128]{2,1,0:T(8,128)S(1)} %get-tuple-element.54), channel_id=1, source_target_pairs={{4,8},{0,12},{8,4},{12,0},{5,9},{1,13},{9,5},{13,1},{6,10},{2,14},... | collective-permute-start | bytes 393224 | tf_op jit(solution)/shard_map/ppermute | solution.py:113
  19.3 11.7 %collective-permute-start.5 = (f32[8,32,128]{2,1,0:T(8,128)S(1)}, f32[8,32,128]{2,1,0:T(8,128)S(1)}, u32[]{:S(2)}, u32[]{:S(2)}) collective-permute-start(f32[8,32,128]{2,1,0:T(8,128)S(1)} %get-tuple-element.55), channel_id=1, source_target_pairs={{0,8},{4,12},{8,0},{12,4},{1,9},{5,13},{9,1},{13,5},{2,10},{6,14},... | collective-permute-start | bytes 393224 | tf_op jit(solution)/shard_map/ppermute | solution.py:113
  20.2 10.8 %collective-permute-start.3 = (f32[8,32,128]{2,1,0:T(8,128)S(1)}, f32[8,32,128]{2,1,0:T(8,128)S(1)}, u32[]{:S(2)}, u32[]{:S(2)}) collective-permute-start(f32[8,32,128]{2,1,0:T(8,128)S(1)} %get-tuple-element.53), channel_id=1, source_target_pairs={{0,4},{8,12},{4,0},{12,8},{1,5},{9,13},{5,1},{13,9},{2,6},{10,14},... | collective-permute-start | bytes 393224 | tf_op jit(solution)/shard_map/ppermute | solution.py:113
  32.8 1.6 %collective-permute-start.6 = (f32[16,32,128]{2,1,0:T(8,128)S(1)}, f32[16,32,128]{2,1,0:T(8,128)S(1)}, u32[]{:S(2)}, u32[]{:S(2)}) collective-permute-start(f32[16,32,128]{2,1,0:T(8,128)S(1)} %get-tuple-element.60), channel_id=1, source_target_pairs={{0,1},{1,0},{2,3},{3,2},{4,5},{5,4},{6,7},{7,6},{8,9},{9,8},{10,11... | collective-permute-start | bytes 786440 | tf_op jit(solution)/shard_map/ppermute | solution.py:397
  34.5 13.6 %collective-permute-start.7 = (f32[16,32,128]{2,1,0:T(8,128)S(1)}, f32[16,32,128]{2,1,0:T(8,128)S(1)}, u32[]{:S(2)}, u32[]{:S(2)}) collective-permute-start(f32[16,32,128]{2,1,0:T(8,128)S(1)} %add.55), channel_id=1, source_target_pairs={{0,2},{1,3},{2,0},{3,1},{4,6},{5,7},{6,4},{7,5},{8,10},{9,11},{10,... | collective-permute-start | bytes 786440 | tf_op jit(solution)/shard_map/ppermute | solution.py:400
  36.0 6.0 %collective-permute-start.10 = (f32[64,64]{1,0:T(8,128)S(1)}, f32[64,64]{1,0:T(8,128)S(1)}, u32[]{:S(2)}, u32[]{:S(2)}) collective-permute-start(f32[64,64]{1,0:T(8,128)S(1)} %gram.1), channel_id=1, source_target_pairs={{0,12},{4,8},{8,4},{12,0},{1,13},{5,9},{9,5},{13,1},{2,14},{6,10},... | collective-permute-start | bytes 49160 | tf_op jit(solution)/shard_map/ppermute | solution.py:132
  37.2 5.4 %collective-permute-start.9 = (f32[64,64]{1,0:T(8,128)S(1)}, f32[64,64]{1,0:T(8,128)S(1)}, u32[]{:S(2)}, u32[]{:S(2)}) collective-permute-start(f32[64,64]{1,0:T(8,128)S(1)} %gram.1), channel_id=1, source_target_pairs={{0,8},{4,12},{8,0},{12,4},{1,9},{5,13},{9,1},{13,5},{2,10},{6,14},... | collective-permute-start | bytes 49160 | tf_op jit(solution)/shard_map/ppermute | solution.py:132
  37.2 5.4 %collective-permute-start.8 = (f32[64,64]{1,0:T(8,128)S(1)}, f32[64,64]{1,0:T(8,128)S(1)}, u32[]{:S(2)}, u32[]{:S(2)}) collective-permute-start(f32[64,64]{1,0:T(8,128)S(1)} %gram.1), channel_id=1, source_target_pairs={{0,4},{4,0},{8,12},{12,8},{1,5},{5,1},{9,13},{13,9},{2,6},{6,2},{1... | collective-permute-start | bytes 49160 | tf_op jit(solution)/shard_map/ppermute | solution.py:132
  48.2 3.6 %collective-permute-start.11 = (f32[16,32,128]{2,1,0:T(8,128)S(1)}, f32[16,32,128]{2,1,0:T(8,128)S(1)}, u32[]{:S(2)}, u32[]{:S(2)}) collective-permute-start(f32[16,32,128]{2,1,0:T(8,128)S(1)} %add.59.refs_3_), channel_id=1, source_target_pairs={{0,1},{1,0},{2,3},{3,2},{4,5},{5,4},{6,7},{7,6},{8,9},{9,8},{10,11... | collective-permute-start | bytes 786440 | tf_op jit(solution)/shard_map/ppermute | solution.py:405
  48.2 5.9 %collective-permute-start.15 = (f32[8,32,128]{2,1,0:T(8,128)S(1)}, f32[8,32,128]{2,1,0:T(8,128)S(1)}, u32[]{:S(2)}, u32[]{:S(2)}) collective-permute-start(f32[8,32,128]{2,1,0:T(8,128)S(1)} %get-tuple-element.68), channel_id=1, source_target_pairs={{0,4},{8,12},{4,0},{12,8},{1,5},{9,13},{5,1},{13,9},{2,6},{10,14},... | collective-permute-start | bytes 393224 | tf_op jit(solution)/shard_map/ppermute | solution.py:113
  50.1 8.2 %collective-permute-start.16 = (f32[8,32,128]{2,1,0:T(8,128)S(1)}, f32[8,32,128]{2,1,0:T(8,128)S(1)}, u32[]{:S(2)}, u32[]{:S(2)}) collective-permute-start(f32[8,32,128]{2,1,0:T(8,128)S(1)} %get-tuple-element.69), channel_id=1, source_target_pairs={{4,8},{0,12},{8,4},{12,0},{5,9},{1,13},{9,5},{13,1},{6,10},{2,14},... | collective-permute-start | bytes 393224 | tf_op jit(solution)/shard_map/ppermute | solution.py:113
  51.2 12.6 %collective-permute-start.17 = (f32[8,32,128]{2,1,0:T(8,128)S(1)}, f32[8,32,128]{2,1,0:T(8,128)S(1)}, u32[]{:S(2)}, u32[]{:S(2)}) collective-permute-start(f32[8,32,128]{2,1,0:T(8,128)S(1)} %get-tuple-element.70), channel_id=1, source_target_pairs={{0,8},{4,12},{8,0},{12,4},{1,9},{5,13},{9,1},{13,5},{2,10},{6,14},... | collective-permute-start | bytes 393224 | tf_op jit(solution)/shard_map/ppermute | solution.py:113
  67.3 8.4 %collective-permute-start.19 = (f32[16,32,128]{2,1,0:T(8,128)S(1)}, f32[16,32,128]{2,1,0:T(8,128)S(1)}, u32[]{:S(2)}, u32[]{:S(2)}) collective-permute-start(f32[16,32,128]{2,1,0:T(8,128)S(1)} %add.60), channel_id=1, source_target_pairs={{0,2},{1,3},{2,0},{3,1},{4,6},{5,7},{6,4},{7,5},{8,10},{9,11},{10,... | collective-permute-start | bytes 786440 | tf_op jit(solution)/shard_map/ppermute | solution.py:400
  75.8 10.7 %collective-permute-start.12 = (f32[8,32,128]{2,1,0:T(8,128)S(1)}, f32[8,32,128]{2,1,0:T(8,128)S(1)}, u32[]{:S(2)}, u32[]{:S(2)}) collective-permute-start(f32[8,32,128]{2,1,0:T(8,128)S(1)} %get-tuple-element.64), channel_id=1, source_target_pairs={{0,4},{8,12},{4,0},{12,8},{1,5},{9,13},{5,1},{13,9},{2,6},{10,14},... | collective-permute-start | bytes 393224 | tf_op jit(solution)/shard_map/ppermute | solution.py:113
  79.9 7.7 %collective-permute-start.23 = (f32[64,128]{1,0:T(8,128)S(1)}, f32[64,128]{1,0:T(8,128)S(1)}, u32[]{:S(2)}, u32[]{:S(2)}) collective-permute-start(f32[64,128]{1,0:T(8,128)S(1)} %cross.1), channel_id=1, source_target_pairs={{0,12},{4,8},{8,4},{12,0},{1,13},{5,9},{9,5},{13,1},{2,14},{6,10},... | collective-permute-start | bytes 98312 | tf_op jit(solution)/shard_map/ppermute | solution.py:132
  80.3 10.3 %collective-permute-start.22 = (f32[64,128]{1,0:T(8,128)S(1)}, f32[64,128]{1,0:T(8,128)S(1)}, u32[]{:S(2)}, u32[]{:S(2)}) collective-permute-start(f32[64,128]{1,0:T(8,128)S(1)} %cross.1), channel_id=1, source_target_pairs={{0,8},{4,12},{8,0},{12,4},{1,9},{5,13},{9,1},{13,5},{2,10},{6,14},... | collective-permute-start | bytes 98312 | tf_op jit(solution)/shard_map/ppermute | solution.py:132
  81.8 9.2 %collective-permute-start.21 = (f32[64,128]{1,0:T(8,128)S(1)}, f32[64,128]{1,0:T(8,128)S(1)}, u32[]{:S(2)}, u32[]{:S(2)}) collective-permute-start(f32[64,128]{1,0:T(8,128)S(1)} %cross.1), channel_id=1, source_target_pairs={{0,4},{4,0},{8,12},{12,8},{1,5},{5,1},{9,13},{13,9},{2,6},{6,2},{1... | collective-permute-start | bytes 98312 | tf_op jit(solution)/shard_map/ppermute | solution.py:132
  84.4 18.8 %collective-permute-start.13 = (f32[8,32,128]{2,1,0:T(8,128)S(1)}, f32[8,32,128]{2,1,0:T(8,128)S(1)}, u32[]{:S(2)}, u32[]{:S(2)}) collective-permute-start(f32[8,32,128]{2,1,0:T(8,128)S(1)} %get-tuple-element.65), channel_id=1, source_target_pairs={{4,8},{0,12},{8,4},{12,0},{5,9},{1,13},{9,5},{13,1},{6,10},{2,14},... | collective-permute-start | bytes 393224 | tf_op jit(solution)/shard_map/ppermute | solution.py:113
  86.5 17.5 %collective-permute-start.14 = (f32[8,32,128]{2,1,0:T(8,128)S(1)}, f32[8,32,128]{2,1,0:T(8,128)S(1)}, u32[]{:S(2)}, u32[]{:S(2)}) collective-permute-start(f32[8,32,128]{2,1,0:T(8,128)S(1)} %get-tuple-element.66), channel_id=1, source_target_pairs={{0,8},{4,12},{8,0},{12,4},{1,9},{5,13},{9,1},{13,5},{2,10},{6,14},... | collective-permute-start | bytes 393224 | tf_op jit(solution)/shard_map/ppermute | solution.py:113
  87.7 18.2 %collective-permute-start.26 = (f32[8,32,128]{2,1,0:T(8,128)S(1)}, f32[8,32,128]{2,1,0:T(8,128)S(1)}, u32[]{:S(2)}, u32[]{:S(2)}) collective-permute-start(f32[8,32,128]{2,1,0:T(8,128)S(1)} %get-tuple-element.86), channel_id=1, source_target_pairs={{0,4},{8,12},{4,0},{12,8},{1,5},{9,13},{5,1},{13,9},{2,6},{10,14},... | collective-permute-start | bytes 393224 | tf_op jit(solution)/shard_map/ppermute | solution.py:113
  90.6 15.3 %collective-permute-start.27 = (f32[8,32,128]{2,1,0:T(8,128)S(1)}, f32[8,32,128]{2,1,0:T(8,128)S(1)}, u32[]{:S(2)}, u32[]{:S(2)}) collective-permute-start(f32[8,32,128]{2,1,0:T(8,128)S(1)} %get-tuple-element.87), channel_id=1, source_target_pairs={{4,8},{0,12},{8,4},{12,0},{5,9},{1,13},{9,5},{13,1},{6,10},{2,14},... | collective-permute-start | bytes 393224 | tf_op jit(solution)/shard_map/ppermute | solution.py:113
  90.9 17.8 %collective-permute-start.28 = (f32[8,32,128]{2,1,0:T(8,128)S(1)}, f32[8,32,128]{2,1,0:T(8,128)S(1)}, u32[]{:S(2)}, u32[]{:S(2)}) collective-permute-start(f32[8,32,128]{2,1,0:T(8,128)S(1)} %get-tuple-element.88), channel_id=1, source_target_pairs={{0,8},{4,12},{8,0},{12,4},{1,9},{5,13},{9,1},{13,5},{2,10},{6,14},... | collective-permute-start | bytes 393224 | tf_op jit(solution)/shard_map/ppermute | solution.py:113
  105.8 5.1 %collective-permute-start.24 = (f32[16,32,128]{2,1,0:T(8,128)S(1)}, f32[16,32,128]{2,1,0:T(8,128)S(1)}, u32[]{:S(2)}, u32[]{:S(2)}) collective-permute-start(f32[16,32,128]{2,1,0:T(8,128)S(1)} %get-tuple-element.85), channel_id=1, source_target_pairs={{0,1},{1,0},{2,3},{3,2},{4,5},{5,4},{6,7},{7,6},{8,9},{9,8},{10,11... | collective-permute-start | bytes 786440 | tf_op jit(solution)/shard_map/ppermute | solution.py:397
  110.9 9.2 %collective-permute-start.25 = (f32[16,32,128]{2,1,0:T(8,128)S(1)}, f32[16,32,128]{2,1,0:T(8,128)S(1)}, u32[]{:S(2)}, u32[]{:S(2)}) collective-permute-start(f32[16,32,128]{2,1,0:T(8,128)S(1)} %add.65), channel_id=1, source_target_pairs={{0,2},{1,3},{2,0},{3,1},{4,6},{5,7},{6,4},{7,5},{8,10},{9,11},{10,... | collective-permute-start | bytes 786440 | tf_op jit(solution)/shard_map/ppermute | solution.py:400
  112.4 12.9 %collective-permute-start.30 = (f32[16,32,128]{2,1,0:T(8,128)S(1)}, f32[16,32,128]{2,1,0:T(8,128)S(1)}, u32[]{:S(2)}, u32[]{:S(2)}) collective-permute-start(f32[16,32,128]{2,1,0:T(8,128)S(1)} %add.67), channel_id=1, source_target_pairs={{0,2},{1,3},{2,0},{3,1},{4,6},{5,7},{6,4},{7,5},{8,10},{9,11},{10,... | collective-permute-start | bytes 786440 | tf_op jit(solution)/shard_map/ppermute | solution.py:400
  120.1 5.3 %collective-permute-start.31 = (f32[16,32,128]{2,1,0:T(8,128)S(1)}, f32[16,32,128]{2,1,0:T(8,128)S(1)}, u32[]{:S(2)}, u32[]{:S(2)}) collective-permute-start(f32[16,32,128]{2,1,0:T(8,128)S(1)} %add.66.refs_0_), channel_id=1, source_target_pairs={{0,1},{1,0},{2,3},{3,2},{4,5},{5,4},{6,7},{7,6},{8,9},{9,8},{10,11... | collective-permute-start | bytes 786440 | tf_op jit(solution)/shard_map/ppermute | solution.py:405
  129.5 6.9 %collective-permute-start.35 = (f32[64,256]{1,0:T(8,128)S(1)}, f32[64,256]{1,0:T(8,128)S(1)}, u32[]{:S(2)}, u32[]{:S(2)}) collective-permute-start(f32[64,256]{1,0:T(8,128)S(1)} %get-tuple-element.96), channel_id=1, source_target_pairs={{0,12},{4,8},{8,4},{12,0},{1,13},{5,9},{9,5},{13,1},{2,14},{6,10},... | collective-permute-start | bytes 196616 | tf_op jit(solution)/shard_map/ppermute | solution.py:132
  130.5 7.6 %collective-permute-start.34 = (f32[64,256]{1,0:T(8,128)S(1)}, f32[64,256]{1,0:T(8,128)S(1)}, u32[]{:S(2)}, u32[]{:S(2)}) collective-permute-start(f32[64,256]{1,0:T(8,128)S(1)} %get-tuple-element.96), channel_id=1, source_target_pairs={{0,8},{4,12},{8,0},{12,4},{1,9},{5,13},{9,1},{13,5},{2,10},{6,14},... | collective-permute-start | bytes 196616 | tf_op jit(solution)/shard_map/ppermute | solution.py:132
  130.5 7.6 %collective-permute-start.33 = (f32[64,256]{1,0:T(8,128)S(1)}, f32[64,256]{1,0:T(8,128)S(1)}, u32[]{:S(2)}, u32[]{:S(2)}) collective-permute-start(f32[64,256]{1,0:T(8,128)S(1)} %get-tuple-element.96), channel_id=1, source_target_pairs={{0,4},{4,0},{8,12},{12,8},{1,5},{5,1},{9,13},{13,9},{2,6},{6,2},{1... | collective-permute-start | bytes 196616 | tf_op jit(solution)/shard_map/ppermute | solution.py:132
  (14 other events, 91.5 us)

commit v2 on v1

--- a/solution.py
+++ b/solution.py
@@ -16,7 +16,7 @@
 
 VMEM = pl.BlockSpec(memory_space=pltpu.VMEM)
 SMEM = pl.BlockSpec(memory_space=pltpu.SMEM)
-ANY = pl.BlockSpec(memory_space=pl.ANY)
+HBM = pl.BlockSpec(memory_space=pltpu.HBM)
 
 
 def contract(a, b, ta=False, tb=False, precision=None):
@@ -128,14 +128,8 @@
         return lax.psum(block, axis)
     step = 1
     while step < size:
-        masks = [step] if step * 2 >= size else [step, 2 * step, 3 * step]
-        got = [lax.ppermute(block, axis, [(i, i ^ mask) for i in range(size)]) for mask in masks]
-        if len(got) == 1:
-            block = block + got[0]
-            step *= 2
-        else:
-            block = (block + got[0]) + (got[1] + got[2])
-            step *= 4
+        block = block + lax.ppermute(block, axis, [(i, i ^ step) for i in range(size)])
+        step *= 2
     return block
 
 
@@ -185,39 +179,46 @@
         [lax.axis_index("vec").reshape(1), table[:, lax.axis_index("res")]]
     ).astype(jnp.int32)
 
-    def own_sum(acc_refs, x_of, split_ref, rows_ref, cols_ref):
+    def own_sum(acc_refs, x_ref, split_ref, rows_ref, cols_ref):
         for s in range(OWN_SLOTS):
             i, j = rows_ref[0, 0, s], cols_ref[0, 0, s]
-            direct = tile_product(x_of(j), split_ref, s, True)
-            mirror = tile_product(x_of(i), split_ref, s, False)
+            direct = tile_product(x_ref[j], split_ref, s, True)
+            mirror = tile_product(x_ref[i], split_ref, s, False)
             for n, acc_ref in enumerate(acc_refs):
                 acc_ref[i] += direct[n * part : (n + 1) * part]
                 acc_ref[j] += mirror[n * part : (n + 1) * part]
 
-    def prepare_body(place_ref, rows_ref, cols_ref, x_ref, diag_ref, tiles_ref, split_ref, a_ref, b_ref, raw_ref, sem):
+    def prepare_body(rows_hbm, cols_hbm, x_hbm, diag_hbm, tiles_hbm, *refs):
+        x_ref, split_ref, a_ref, b_ref, rows_ref, cols_ref, diag_ref, raw_ref, sem = refs
         size = slots // 4
         copies = [
+            pltpu.make_async_copy(src, dst, sem.at[n])
+            for n, (src, dst) in enumerate(
+                [(x_hbm, x_ref), (diag_hbm, diag_ref), (rows_hbm, rows_ref), (cols_hbm, cols_ref)]
+            )
+        ]
+        tile_copies = [
             pltpu.make_async_copy(
-                tiles_ref.at[0, 0, pl.ds(n * size, size)], raw_ref.at[pl.ds(n * size, size)], sem.at[n]
+                tiles_hbm.at[0, 0, pl.ds(n * size, size)], raw_ref.at[pl.ds(n * size, size)], sem.at[4 + n]
             )
             for n in range(4)
         ]
+        for c in copies + tile_copies:
+            c.start()
+        for n in range(4):
+            tile_copies[n].wait()
+            for s in range(n * size, (n + 1) * size):
+                split_ref[s, 0], split_ref[s, 1] = pieces(raw_ref[s], 2)
         for c in copies:
-            c.start()
-        first = (place_ref[0] == 0).astype(F32)
+            c.wait()
+        first = (lax.axis_index("vec") == 0).astype(F32)
         d = ((diag_ref[...] - SHIFT) * first)[:, None, :]
         a_ref[...] = x_ref[:, :part] * d
         b_ref[...] = x_ref[:, part:] * d
-        for n in range(4):
-            copies[n].wait()
-            for s in range(n * size, (n + 1) * size):
-                split_ref[s, 0], split_ref[s, 1] = pieces(raw_ref[s], 2)
-        own_sum([a_ref, b_ref], lambda i: x_ref[i], split_ref, rows_ref, cols_ref)
-
-    def own_body(place_ref, rows_ref, cols_ref, x_ref, diag_ref, split_ref, acc_ref):
-        first = (place_ref[0] == 0).astype(F32)
-        acc_ref[...] = x_ref[...] * ((diag_ref[...] - SHIFT) * first)[:, None, :]
-        own_sum([acc_ref], lambda i: x_ref[i], split_ref, rows_ref, cols_ref)
+        own_sum([a_ref, b_ref], x_ref, split_ref, rows_ref, cols_ref)
+
+    def own_body(rows_ref, cols_ref, x_ref, split_ref, prior_ref, acc_ref):
+        own_sum([acc_ref], x_ref, split_ref, rows_ref, cols_ref)
 
     def pack(place_ref, rows_ref, counts_ref, asked_refs, x_ref, split_ref, outs):
         for p in range(count):
@@ -254,26 +255,25 @@
 
     def resend_body(place_ref, rows_ref, counts_ref, *refs):
         asked_refs = refs[:count]
-        mine_ref, other_ref, split_ref, y_ref = refs[count : count + 4]
-        outs = refs[count + 4 :]
+        mine_ref, other_ref, diag_ref, split_ref, y_ref, acc_ref = refs[count : count + 6]
+        outs = refs[count + 6 :]
         settle(place_ref, mine_ref, other_ref, y_ref)
         pack(
             place_ref, rows_ref, counts_ref, asked_refs, y_ref, split_ref,
             [(outs[p],) for p in range(count)],
         )
-
-    def join_body(place_ref, rows_ref, counts_ref, *refs):
-        asked_refs, got_refs = refs[:count], refs[count : 2 * count]
-        split_ref, part_ref, keep_ref, give_ref, acc_ref = refs[2 * count :]
-        acc_ref[...] = part_ref[...]
-        for p in range(count):
+        first = (place_ref[0] == 0).astype(F32)
+        acc_ref[...] = y_ref[...] * ((diag_ref[...] - SHIFT) * first)[:, None, :]
+
+    def join_rounds(members, place_ref, rows_ref, counts_ref, asked_refs, got_refs, split_ref, acc_ref):
+        for n, p in enumerate(members):
             role = place_ref[1 + p]
 
             @pl.when(role > 0)
             def _():
                 base = OWN_SLOTS + (role - 1) * CAP
                 for c in range(CAP):
-                    term = tile_product(got_refs[p][c], split_ref, base + c, True)
+                    term = tile_product(got_refs[n][c], split_ref, base + c, True)
                     acc_ref[rows_ref[0, 0, base + c]] += jnp.where(
                         c < counts_ref[0, 0, role - 1], term, 0.0
                     )
@@ -282,11 +282,39 @@
             def _():
                 base = OWN_SLOTS + (-role - 1) * CAP
                 for c in range(CAP):
-                    acc_ref[asked_refs[p][0, 0, base + c]] += got_refs[p][c]
-
-        core = place_ref[0] % 2
-        keep_ref[...] = acc_ref[pl.ds(core * half, half)]
-        give_ref[...] = acc_ref[pl.ds((1 - core) * half, half)]
+                    acc_ref[asked_refs[n][0, 0, base + c]] += got_refs[n][c]
+
+    def join(acc, got, members, last=False):
+        size = len(members)
+
+        def body(place_ref, rows_ref, counts_ref, *refs):
+            asked_refs, got_refs = refs[:size], refs[size : 2 * size]
+            split_ref, prior_ref = refs[2 * size : 2 * size + 2]
+            outs = refs[2 * size + 2 :]
+            if last:
+                keep_ref, give_ref, acc_ref = outs
+                acc_ref[...] = prior_ref[...]
+            else:
+                (acc_ref,) = outs
+            join_rounds(
+                members, place_ref, rows_ref, counts_ref, asked_refs, got_refs, split_ref, acc_ref
+            )
+            if last:
+                core = place_ref[0] % 2
+                keep_ref[...] = acc_ref[pl.ds(core * half, half)]
+                give_ref[...] = acc_ref[pl.ds((1 - core) * half, half)]
+
+        out = call(
+            body,
+            [halfchunk] * 2 if last else [chunk],
+            [SMEM] * (3 + size) + [VMEM] * (size + 2),
+            [pltpu.VMEM(chunk, F32)] if last else [],
+            name="join",
+            aliases=None if last else {3 + 2 * size + 1: 0},
+        )(
+            place, tile_rows, slot_counts, *[asked[p] for p in members], *[got[p] for p in members], split, acc
+        )
+        return out if last else out[0]
 
     def gram_body(x_ref, out_ref):
         total = jnp.zeros(square, F32)
@@ -321,49 +349,45 @@
         back = -dot(dot(inverse, cross), start_inv)
         gain_ref[...] = gain
         coef_ref[:width, :width] = -dot(lower, start_inv)
-        coef_ref[:width, width:] = back
+        coef_ref[:width, width : 2 * width] = back
+        coef_ref[:width, 2 * width :] = gain
         coef_ref[width:, :width] = back
-        coef_ref[width:, width:] = gain
-
-    def blend_body(x_ref, a_ref, b_ref, coef_ref, w_ref, q_ref, out_ref):
+        coef_ref[width:, width : 2 * width] = gain
+        coef_ref[width:, 2 * width :] = jnp.zeros(square, F32)
+
+    def blend_body(place_ref, x_ref, a_ref, b_ref, mine_ref, other_ref, coef_ref, w_ref, q_ref, out_ref, z_ref):
+        settle(place_ref, mine_ref, other_ref, z_ref)
         total = jnp.zeros(square, F32)
         for n in range(0, rows, 2):
             qs = []
             stacks = [
-                jnp.concatenate([x_ref[m], a_ref[m], b_ref[m]], axis=0) for m in (n, n + 1)
+                jnp.concatenate([x_ref[m], a_ref[m], b_ref[m], z_ref[m]], axis=0) for m in (n, n + 1)
             ]
-            for m, both in zip((n, n + 1), wide_product(coef_ref[...], stacks)):
+            for m, both in zip((n, n + 1), wide_product(coef_ref[:, : 2 * width + part], stacks)):
                 w_ref[m] = both[:width]
                 q_ref[m] = both[width:]
                 qs.append(both[width:])
             total += gram_step(qs, [qs])
         out_ref[...] = total
 
-    def third_body(place_ref, *refs):
-        mine_refs, other_refs = refs[0:2], refs[2:4]
-        prior_ref, q_ref, gain_ref, norm_ref, w_ref, out_ref = refs[4:10]
-        z_refs = refs[10:12]
-        for n in range(2):
-            settle(place_ref, mine_refs[n], other_refs[n], z_refs[n])
+    def third_body(place_ref, mine_ref, other_ref, prior_ref, q_ref, gain_ref, w_ref, out_ref, z_ref):
+        settle(place_ref, mine_ref, other_ref, z_ref)
         total = jnp.zeros((width, 2 * width), F32)
         for n in range(0, rows, 2):
-            zs = [jnp.concatenate([z_refs[0][m], z_refs[1][m]], axis=0) for m in (n, n + 1)]
             ws = []
-            for m, w in zip((n, n + 1), wide_product(gain_ref[...], zs)):
+            for m, w in zip((n, n + 1), wide_product(gain_ref[:, part:], [z_ref[n], z_ref[n + 1]])):
                 w = w + prior_ref[m]
                 w_ref[m] = w
                 ws.append(w)
             total += gram_step(ws, [[q_ref[n], q_ref[n + 1]], ws])
-        out_ref[:, : 2 * width] = total
-        out_ref[:, 2 * width : 3 * width] = norm_ref[...]
-        out_ref[:, 3 * width :] = jnp.zeros(square, F32)
-
-    def fourth_body(gram_ref, cross_ref, lower_ref, coef_ref):
+        out_ref[...] = total
+
+    def fourth_body(gram_ref, norm_ref, cross_ref, lower_ref, coef_ref):
         cross = gram_ref[:, :width]
-        norm = gram_ref[:, 2 * width : 3 * width]
+        norm = norm_ref[...]
         taken = cross + SHIFT * (norm - identity())
         mixed = dot(taken, cross, tb=True)
-        squared = gram_ref[:, width : 2 * width] - mixed - mixed.T + dot(dot(taken, norm), taken, tb=True)
+        squared = gram_ref[:, width:] - mixed - mixed.T + dot(dot(taken, norm), taken, tb=True)
         upper, inverse = factor(squared)
         cross_ref[...] = taken + SHIFT * identity()
         lower_ref[...] = upper.T
@@ -380,93 +404,116 @@
                 out_ref[m] = out
 
     swap = [(i, i ^ 1) for i in range(lanes)]
+    cuts = [count * n // 3 for n in range(4)]
+    groups = [list(range(cuts[n], cuts[n + 1])) for n in range(3)]
 
     def spread(sent):
         return [exchange(s, "res", entry["pairs"]) for s, entry in zip(sent, rounds)]
 
-    def join(got, prior, token):
-        return call(
-            join_body,
-            [halfchunk] * 2,
-            [SMEM] * (3 + count) + [VMEM] * (count + 2),
-            [pltpu.VMEM(chunk, F32)],
-            name="join",
-        )(place, tile_rows, slot_counts, *asked, *got, split, after(prior, token))
-
-    def vec_sum(keep, give, token=None):
-        mine = keep + lax.ppermute(give, "vec", swap)
+    def across(mine, *tokens):
         step = 2
         while step < lanes:
             got = lax.ppermute(mine, "vec", [(i, i ^ step) for i in range(lanes)])
-            if token is not None:
-                got = after(got, token)
-            mine = mine + got
+            mine = mine + after(got, *tokens)
             step *= 2
-        return mine, lax.ppermute(mine, "vec", swap)
-
-    def resend(mine, other, token):
-        y, *sent = call(
-            resend_body, [chunk] + [packet] * count, [SMEM] * (3 + count) + [VMEM] * 3, name="resend"
-        )(place, tile_rows, slot_counts, *asked, mine, after(other, token), split)
-        return y, sent
-
-    def own(y, token):
-        (acc,) = call(own_body, [chunk], [SMEM] * 3 + [VMEM] * 3, name="own")(
-            place, tile_rows, tile_cols, after(y, token), diagonal, split
-        )
-        return acc
+        return mine
+
+    def resend(mine, other):
+        y, acc, *sent = call(
+            resend_body,
+            [chunk, chunk] + [packet] * count,
+            [SMEM] * (3 + count) + [VMEM] * 4,
+            name="resend",
+        )(place, tile_rows, slot_counts, *asked, mine, other, diagonal, split)
+        return y, acc, spread(sent)
+
+    def own(acc, y):
+        return call(own_body, [chunk], [SMEM] * 2 + [VMEM] * 3, name="own", aliases={4: 0})(
+            tile_rows, tile_cols, y, split, acc
+        )[0]
 
     asked = [exchange(tile_cols, "res", entry["pairs"]) for entry in rounds]
-    split, prior_a, prior_b = call(
+    x, split, acc_a, acc_b = call(
         prepare_body,
-        [split_shape, chunk, chunk],
-        [SMEM] * 3 + [VMEM] * 2 + [ANY],
-        [pltpu.VMEM((slots, length, length), F32), pltpu.SemaphoreType.DMA((4,))],
+        [full, split_shape, chunk, chunk],
+        [HBM] * 5,
+        [
+            pltpu.SMEM(tile_rows.shape, jnp.int32),
+            pltpu.SMEM(tile_cols.shape, jnp.int32),
+            pltpu.VMEM(diagonal.shape, F32),
+            pltpu.VMEM((slots, length, length), F32),
+            pltpu.SemaphoreType.DMA((8,)),
+        ],
         name="prepare",
-    )(place, tile_rows, tile_cols, start_block, diagonal, hess_tiles)
+    )(tile_rows, tile_cols, start_block, diagonal, hess_tiles)
     sent = call(
         send_body, [packet] * (2 * count), [SMEM] * (3 + count) + [VMEM] * 2, name="send"
-    )(place, tile_rows, slot_counts, *asked, start_block, split)
+    )(place, tile_rows, slot_counts, *asked, x, split)
     got_a = spread(sent[:count])
     got_b = spread(sent[count:])
-    (start_gram,) = call(gram_body, [square], [VMEM], name="gram")(after(start_block, sent[0]))
-    start_total = all_sum(start_gram, "res")
-    keep, give = join(got_a, prior_a, start_gram)
-    (start_inv,) = call(first_body, [square], [VMEM], name="first")(after(start_total, keep))
-    mine, other = vec_sum(keep, give, start_inv)
-    y_a, sent = resend(mine, other, start_inv)
-    got_a = spread(sent)
-    keep, give = join(got_b, prior_b, y_a)
-    prior_a = own(y_a, keep)
-    mine, other = vec_sum(keep, give, prior_a)
-    y_b, sent = resend(mine, other, prior_a)
-    got_b = spread(sent)
-    (cross_gram,) = call(cross_body, [(width, 2 * width)], [VMEM] * 3, name="cross")(
-        start_block, y_a, y_b
-    )
-    cross_total = all_sum(cross_gram, "res")
-    prior_b = own(y_b, cross_gram)
+    (gram,) = call(gram_body, [square], [VMEM], name="gram")(after(x, sent[0]))
+    start_gram = all_sum(gram, "res")
+    for n in range(2):
+        acc_a = join(after(acc_a, gram), got_a, groups[n])
+    keep_a, give_a = join(acc_a, got_a, groups[2], last=True)
+
+    core = lax.ppermute(give_a, "vec", swap)
+    acc_b = join(acc_b, got_b, groups[0])
+    mine_a = keep_a + after(core, acc_b)
+    (start_inv,) = call(first_body, [square], [VMEM], name="first")(after(start_gram, mine_a))
+    acc_b = join(after(acc_b, start_inv), got_b, groups[1])
+    mine_a = across(mine_a, acc_b)
+    other_a = lax.ppermute(mine_a, "vec", swap)
+    keep_b, give_b = join(acc_b, got_b, groups[2], last=True)
+    y_a, acc_a, got_a = resend(mine_a, after(other_a, keep_b))
+
+    core = lax.ppermute(give_b, "vec", swap)
+    acc_a = join(acc_a, got_a, groups[0])
+    mine_b = keep_b + after(core, acc_a)
+    acc_a = own(after(acc_a, mine_b), y_a)
+    acc_a = join(acc_a, got_a, groups[1])
+    mine_b = across(mine_b, acc_a)
+    other_b = lax.ppermute(mine_b, "vec", swap)
+    keep_a, give_a = join(acc_a, got_a, groups[2], last=True)
+    y_b, acc_b, got_b = resend(mine_b, after(other_b, keep_a))
+
+    (gram,) = call(cross_body, [(width, 2 * width)], [VMEM] * 3, name="cross")(x, y_a, y_b)
+    core = lax.ppermute(give_a, "vec", swap)
+    acc_b = own(after(acc_b, gram), y_b)
+    acc_b = join(acc_b, got_b, groups[0])
+    mine_a = keep_a + after(core, acc_b)
+    cross_gram = all_sum(gram, "res")
     cross1, lower1, coef, gain = call(
-        second_body, [square, square, (2 * width, 2 * width), square], [VMEM] * 2, name="second"
-    )(after(cross_total, prior_b), start_inv)
-    w_prior, q, norm = call(blend_body, [full, full, square], [VMEM] * 4, name="blend")(
-        start_block, y_a, y_b, coef
-    )
-    keep_a, give_a = join(got_a, prior_a, norm)
-    mine_a, other_a = vec_sum(keep_a, give_a)
-    keep_b, give_b = join(got_b, prior_b, keep_a)
-    mine_b, other_b = vec_sum(keep_b, give_b)
+        second_body, [square, square, (2 * width, 3 * width), square], [VMEM] * 2, name="second"
+    )(after(cross_gram, mine_a), start_inv)
+    acc_b = join(after(acc_b, gain), got_b, groups[1])
+    mine_a = across(mine_a, acc_b)
+    other_a = lax.ppermute(mine_a, "vec", swap)
+    keep_b, give_b = join(acc_b, got_b, groups[2], last=True)
+
+    core = lax.ppermute(give_b, "vec", swap)
+    mine_b = keep_b + core
+    w_prior, q, norm = call(
+        blend_body,
+        [full, full, square],
+        [SMEM] + [VMEM] * 6,
+        [pltpu.VMEM(chunk, F32)],
+        name="blend",
+    )(place, x, y_a, y_b, mine_a, other_a, after(coef, mine_b))
+    mine_b = across(mine_b, norm)
+    other_b = lax.ppermute(mine_b, "vec", swap)
     w, gram = call(
         third_body,
-        [full, (width, 4 * width)],
-        [SMEM] + [VMEM] * 8,
-        [pltpu.VMEM(chunk, F32)] * 2,
+        [full, (width, 2 * width)],
+        [SMEM] + [VMEM] * 5,
+        [pltpu.VMEM(chunk, F32)],
         name="third",
-    )(place, mine_a, mine_b, other_a, other_b, w_prior, q, gain, norm)
+    )(place, mine_b, other_b, w_prior, q, gain)
+    norm = all_sum(norm, "res")
     gram = all_sum(gram, "res")
     cross2, lower2, coef = call(
-        fourth_body, [square, square, (width, 2 * width)], [VMEM], name="fourth"
-    )(gram)
+        fourth_body, [square, square, (width, 2 * width)], [VMEM] * 2, name="fourth"
+    )(gram, norm)
     return call(last_body, [full, (4, width, width)], [VMEM] * 7, name="last")(
         w, q, coef, cross1, lower1, cross2, lower2
     )

time: 147 us -> 160 us (1.088)
  waiting for transfers between devices: 54.3 us -> 68.7 us
  starting transfers between devices: 37.1 us -> 30.3 us
  Pallas kernels: 48 us -> 53.2 us
    ppermute x15, waiting for transfers between devices: 23.1 us -> 43.1 us  [exchange(): lax.ppermute(block, axis, [(a, b) for a, b in pairs] + [(b, a) for a, b i...]
    ppermute x21 -> x20, waiting for transfers between devices: 31.2 us -> 25.6 us  [the longest x8 21 us: all_sum(): lax.ppermute(block, axis, [(i, i ^ step) for i in range(size)])]
    pallas_call x15 -> x23, Pallas kernels: 43.3 us -> 48.5 us  [the longest x12 11.7 us: join(): call(body, [halfchunk] * 2 if last else [chunk], [SMEM] * (3 + size) + [V...]
    ppermute x15, starting transfers between devices: 19.7 us -> 16.1 us  [exchange(): lax.ppermute(block, axis, [(a, b) for a, b in pairs] + [(b, a) for a, b i...]
    ppermute x21 -> x20, starting transfers between devices: 17.3 us -> 14.2 us  [the longest x8 8.86 us: all_sum(): lax.ppermute(block, axis, [(i, i ^ step) for i in range(size)])]
    unnamed x20 -> x18, local copies, waits for them, and re-layouts: 5.09 us -> 5.09 us
  transfers between devices with their start and end apart: 36 -> 35, of which waited for: 19 -> 18; matrix products, arithmetic and copies ran while one was open for 1% -> 1% of each run, Pallas kernels for 22% -> 25%
where the time goes in v2:
time: 160 us; the launch traced here: 159 us
  waiting for transfers between devices  68.7 us (43%)
  Pallas kernels  53.2 us (33%)
  starting transfers between devices  30.3 us (19%)
  local copies, waits for them, and re-layouts  5.77 us (4%)
    ppermute x15, waiting for transfers between devices, exchange(): lax.ppermute(block, axis, [(a, b) for a, b in pairs] + [(b, a) for a, b i...  43.1 us
    ppermute x8, waiting for transfers between devices, all_sum(): lax.ppermute(block, axis, [(i, i ^ step) for i in range(size)])  21 us
    ppermute x15, starting transfers between devices, exchange(): lax.ppermute(block, axis, [(a, b) for a, b in pairs] + [(b, a) for a, b i...  16.1 us
    pallas_call x12, Pallas kernels, join(): call(body, [halfchunk] * 2 if last else [chunk], [SMEM] * (3 + size) + [V...  11.7 us
    ppermute x8, starting transfers between devices, all_sum(): lax.ppermute(block, axis, [(i, i ^ step) for i in range(size)])  8.86 us
    pallas_call x1, Pallas kernels, local(): call(second_body, [square, square, (2 * width, 3 * width), square], [VMEM...  6.47 us
    pallas_call x1, Pallas kernels, local(): call(fourth_body, [square, square, (width, 2 * width)], [VMEM] * 2, name=...  6.25 us
    pallas_call x1, Pallas kernels, local(): call(blend_body, [full, full, square], [SMEM] + [VMEM] * 6, [pltpu.VMEM(c...  5.72 us
  transfers between devices with their start and end apart: 35, of which 18 were waited for; matrix products, arithmetic and copies ran while one was open for 1% of the time, Pallas kernels for 25%

profile of v2, /device:TPU:0, one launch (start us, length us, event | category | flops | bytes accessed | tf_op | source)
XLA Modules:
  0.0 159.5 jit_solution(9021271673588318702)
XLA Ops:
  0.6 5.1 %collective-permute-start.2 = (s32[1,1,44]{2,1,0:T(1,128)}, s32[1,1,44]{2,1,0:T(1,128)S(1)}, u32[]{:S(2)}, u32[]{:S(2)}) collective-permute-start(s32[1,1,44]{2,1,0:T(1,128)} %cols_ref.3), channel_id=1, source_target_pairs={{4,8},{0,12},{8,4},{12,0},{5,9},{1,13},{9,5},{13,1},{6,10},{2,14},... | collective-permute-start | bytes 536 | tf_op jit(solution)/shard_map/ppermute | solution.py:113
  7.2 1.8 %copy-done = f32[1,1,44,128,128]{4,3,2,1,0:T(8,128)S(1)} copy-done((f32[1,1,44,128,128]{4,3,2,1,0:T(8,128)S(1)}, f32[1,1,44,128,128]{4,3,2,1,0:T(8,128)}, u32[]{:S(2)}) %copy-start) | copy-done | bytes 2883608
  12.2 3.1 %prepare.1 = (f32[32,64,128]{2,1,0:T(8,128)S(1)}, bf16[44,2,128,128]{3,2,1,0:T(8,128)(2,1)S(1)}, f32[32,32,128]{2,1,0:T(8,128)S(1)}, f32[32,32,128]{2,1,0:T(8,128)S(1)}) custom-call(s32[1,1,44]{2,1,0:T(1,128)S(1)} %copy-done.2, s32[1,1,44]{2,1,0:T(1,128)S(1)} %copy-done.7, f32[32,64,128]{2,1,0:T(8,128)S(1)} %copy-done.1, f32[32,128]{1,0:T(8,128)S(1)} %copy-done.4, ...), custom_call_target="tpu_custom_call" | custom-call | tf_op jit(solution)/shard_map/prepare/pallas_call | solution.py:436
  18.1 2.1 %collective-permute-start.9 = (f32[8,32,128]{2,1,0:T(8,128)S(1)}, f32[8,32,128]{2,1,0:T(8,128)S(1)}, u32[]{:S(2)}, u32[]{:S(2)}) collective-permute-start(f32[8,32,128]{2,1,0:T(8,128)S(1)} %get-tuple-element.70), channel_id=1, source_target_pairs={{4,8},{0,12},{8,4},{12,0},{5,9},{1,13},{9,5},{13,1},{6,10},{2,14},... | collective-permute-start | bytes 393224 | tf_op jit(solution)/shard_map/ppermute | solution.py:113
  21.0 1.8 %collective-permute-done.10.refs_1_ = f32[8,32,128]{2,1,0:T(8,128)S(1)} collective-permute-done((f32[8,32,128]{2,1,0:T(8,128)S(1)}, f32[8,32,128]{2,1,0:T(8,128)S(1)}, u32[]{:S(2)}, u32[]{:S(2)}) %collective-permute-start.10) | collective-permute-done | bytes 131104 | tf_op jit(solution)/shard_map/ppermute | solution.py:113
  23.8 3.4 %collective-permute-done.9.refs_1_ = f32[8,32,128]{2,1,0:T(8,128)S(1)} collective-permute-done((f32[8,32,128]{2,1,0:T(8,128)S(1)}, f32[8,32,128]{2,1,0:T(8,128)S(1)}, u32[]{:S(2)}, u32[]{:S(2)}) %collective-permute-start.9) | collective-permute-done | bytes 131104 | tf_op jit(solution)/shard_map/ppermute | solution.py:113
  28.1 3.3 %collective-permute-done.8.refs_1_ = f32[8,32,128]{2,1,0:T(8,128)S(1)} collective-permute-done((f32[8,32,128]{2,1,0:T(8,128)S(1)}, f32[8,32,128]{2,1,0:T(8,128)S(1)}, u32[]{:S(2)}, u32[]{:S(2)}) %collective-permute-start.8) | collective-permute-done | bytes 131104 | tf_op jit(solution)/shard_map/ppermute | solution.py:113
  32.6 5.8 %collective-permute-done.5.refs_1_ = f32[8,32,128]{2,1,0:T(8,128)S(1)} collective-permute-done((f32[8,32,128]{2,1,0:T(8,128)S(1)}, f32[8,32,128]{2,1,0:T(8,128)S(1)}, u32[]{:S(2)}, u32[]{:S(2)}) %collective-permute-start.5) | collective-permute-done | bytes 131104 | tf_op jit(solution)/shard_map/ppermute | solution.py:113
  41.1 1.8 %collective-permute-start.4 = (f32[8,32,128]{2,1,0:T(8,128)S(1)}, f32[8,32,128]{2,1,0:T(8,128)S(1)}, u32[]{:S(2)}, u32[]{:S(2)}) collective-permute-start(f32[8,32,128]{2,1,0:T(8,128)S(1)} %get-tuple-element.64), channel_id=1, source_target_pairs={{4,8},{0,12},{8,4},{12,0},{5,9},{1,13},{9,5},{13,1},{6,10},{2,14},... | collective-permute-start | bytes 393224 | tf_op jit(solution)/shard_map/ppermute | solution.py:113
  42.8 4.9 %collective-permute-done.6 = f32[64,64]{1,0:T(8,128)S(1)} collective-permute-done((f32[64,64]{1,0:T(8,128)S(1)}, f32[64,64]{1,0:T(8,128)S(1)}, u32[]{:S(2)}, u32[]{:S(2)}) %collective-permute-start.6) | collective-permute-done | bytes 16416 | tf_op jit(solution)/shard_map/ppermute | solution.py:131
  49.0 3.9 %collective-permute-done.7 = f32[64,64]{1,0:T(8,128)S(1)} collective-permute-done((f32[64,64]{1,0:T(8,128)S(1)}, f32[64,64]{1,0:T(8,128)S(1)}, u32[]{:S(2)}, u32[]{:S(2)}) %collective-permute-start.7) | collective-permute-done | bytes 16416 | tf_op jit(solution)/shard_map/ppermute | solution.py:131
  52.9 5.5 %first.1.inverse_ref = f32[64,64]{1,0:T(8,128)S(1)} custom-call(f32[64,64]{1,0:T(8,128)S(1)} %add.53.gram_ref), custom_call_target="tpu_custom_call" | custom-call | tf_op jit(solution)/shard_map/first/pallas_call | solution.py:463
  60.2 8.8 %collective-permute-done.3.refs_1_ = f32[8,32,128]{2,1,0:T(8,128)S(1)} collective-permute-done((f32[8,32,128]{2,1,0:T(8,128)S(1)}, f32[8,32,128]{2,1,0:T(8,128)S(1)}, u32[]{:S(2)}, u32[]{:S(2)}) %collective-permute-start.3) | collective-permute-done | bytes 131104 | tf_op jit(solution)/shard_map/ppermute | solution.py:113
  71.7 5.8 %collective-permute-done.15.refs_1_ = f32[8,32,128]{2,1,0:T(8,128)S(1)} collective-permute-done((f32[8,32,128]{2,1,0:T(8,128)S(1)}, f32[8,32,128]{2,1,0:T(8,128)S(1)}, u32[]{:S(2)}, u32[]{:S(2)}) %collective-permute-start.15) | collective-permute-done | bytes 131104 | tf_op jit(solution)/shard_map/ppermute | solution.py:113
  79.3 1.7 %own.2.refs_3_ = f32[32,32,128]{2,1,0:T(8,128)S(1)} custom-call(s32[1,1,44]{2,1,0:T(1,128)S(1)} %copy-done.3, s32[1,1,44]{2,1,0:T(1,128)S(1)} %copy-done.8, f32[32,32,128]{2,1,0:T(8,128)S(1)} %get-tuple-element.87.x_ref.a_ref, bf16[44,2,128,128]{3,2,1,0:T(8,128)(2,1)S(1)} %get-tuple-element.62.refs_4_.refs_2_.refs_6_.split_ref, ...), custom_call_target="tpu_custom_call", output_to_operand_aliasing={{}: (4, {})} | custom-call | tf_op jit(solution)/shard_map/own/pallas_call | solution.py:431
  81.1 4.8 %collective-permute-done.17.refs_1_ = f32[8,32,128]{2,1,0:T(8,128)S(1)} collective-permute-done((f32[8,32,128]{2,1,0:T(8,128)S(1)}, f32[8,32,128]{2,1,0:T(8,128)S(1)}, u32[]{:S(2)}, u32[]{:S(2)}) %collective-permute-start.17) | collective-permute-done | bytes 131104 | tf_op jit(solution)/shard_map/ppermute | solution.py:113
  87.3 9.3 %collective-permute-done.19.refs_1_ = f32[8,32,128]{2,1,0:T(8,128)S(1)} collective-permute-done((f32[8,32,128]{2,1,0:T(8,128)S(1)}, f32[8,32,128]{2,1,0:T(8,128)S(1)}, u32[]{:S(2)}, u32[]{:S(2)}) %collective-permute-start.19) | collective-permute-done | bytes 131104 | tf_op jit(solution)/shard_map/ppermute | solution.py:113
  99.6 3.3 %collective-permute-start.20 = (f32[8,32,128]{2,1,0:T(8,128)S(1)}, f32[8,32,128]{2,1,0:T(8,128)S(1)}, u32[]{:S(2)}, u32[]{:S(2)}) collective-permute-start(f32[8,32,128]{2,1,0:T(8,128)S(1)} %get-tuple-element.93), channel_id=1, source_target_pairs={{0,8},{4,12},{8,0},{12,4},{1,9},{5,13},{9,1},{13,5},{2,10},{6,14},... | collective-permute-start | bytes 393224 | tf_op jit(solution)/shard_map/ppermute | solution.py:113
  104.9 4.5 %collective-permute-done.23 = f32[64,128]{1,0:T(8,128)S(1)} collective-permute-done((f32[64,128]{1,0:T(8,128)S(1)}, f32[64,128]{1,0:T(8,128)S(1)}, u32[]{:S(2)}, u32[]{:S(2)}) %collective-permute-start.23) | collective-permute-done | bytes 32800 | tf_op jit(solution)/shard_map/ppermute | solution.py:131
  109.4 1.8 %collective-permute-start.24 = (f32[64,128]{1,0:T(8,128)S(1)}, f32[64,128]{1,0:T(8,128)S(1)}, u32[]{:S(2)}, u32[]{:S(2)}) collective-permute-start(f32[64,128]{1,0:T(8,128)S(1)} %add.58), channel_id=1, source_target_pairs={{0,8},{4,12},{8,0},{12,4},{1,9},{5,13},{9,1},{13,5},{2,10},{6,14},... | collective-permute-start | bytes 98312 | tf_op jit(solution)/shard_map/ppermute | solution.py:131
  111.3 1.7 %own.3.refs_3_ = f32[32,32,128]{2,1,0:T(8,128)S(1)} custom-call(s32[1,1,44]{2,1,0:T(1,128)S(1)} %copy-done.3, s32[1,1,44]{2,1,0:T(1,128)S(1)} %copy-done.8, f32[32,32,128]{2,1,0:T(8,128)S(1)} %get-tuple-element.96.b_ref.x_ref, bf16[44,2,128,128]{3,2,1,0:T(8,128)(2,1)S(1)} %get-tuple-element.62.refs_4_.refs_2_.refs_6_.split_ref, ...), custom_call_target="tpu_custom_call", output_to_operand_aliasing={{}: (4, {})} | custom-call | tf_op jit(solution)/shard_map/own/pallas_call | solution.py:431
  113.0 3.3 %collective-permute-done.24 = f32[64,128]{1,0:T(8,128)S(1)} collective-permute-done((f32[64,128]{1,0:T(8,128)S(1)}, f32[64,128]{1,0:T(8,128)S(1)}, u32[]{:S(2)}, u32[]{:S(2)}) %collective-permute-start.24) | collective-permute-done | bytes 32800 | tf_op jit(solution)/shard_map/ppermute | solution.py:131
  119.0 6.5 %second.1 = (f32[64,64]{1,0:T(8,128)S(1)}, f32[64,64]{1,0:T(8,128)S(1)}, f32[128,192]{1,0:T(8,128)S(1)}, f32[64,64]{1,0:T(8,128)S(1)}) custom-call(f32[64,128]{1,0:T(8,128)S(1)} %add.59.gram_ref, f32[64,64]{1,0:T(8,128)S(1)} %first.1.inverse_ref), custom_call_target="tpu_custom_call" | custom-call | tf_op jit(solution)/shard_map/second/pallas_call | solution.py:486
  129.6 5.7 %blend.1 = (f32[32,64,128]{2,1,0:T(8,128)S(1)}, f32[32,64,128]{2,1,0:T(8,128)S(1)}, f32[64,64]{1,0:T(8,128)S(1)}) custom-call(s32[4]{0:T(128)S(1)} %pad_add_fusion.place_ref, f32[32,64,128]{2,1,0:T(8,128)S(1)} %get-tuple-element.68.refs_3_.x_ref, f32[32,32,128]{2,1,0:T(8,128)S(1)} %get-tuple-element.87.x_ref.a_ref, ...), custom_call_target="tpu_custom_call" | custom-call | tf_op jit(solution)/shard_map/blend/pallas_call | solution.py:496
  135.3 2.2 %collective-permute-done.27 = f32[16,32,128]{2,1,0:T(8,128)S(1)} collective-permute-done((f32[16,32,128]{2,1,0:T(8,128)S(1)}, f32[16,32,128]{2,1,0:T(8,128)S(1)}, u32[]{:S(2)}, u32[]{:S(2)}) %collective-permute-start.27) | collective-permute-done | bytes 262176 | tf_op jit(solution)/shard_map/ppermute | solution.py:416
  139.2 2.6 %third.1 = (f32[32,64,128]{2,1,0:T(8,128)S(1)}, f32[64,128]{1,0:T(8,128)S(1)}) custom-call(s32[4]{0:T(128)S(1)} %pad_add_fusion.place_ref, f32[16,32,128]{2,1,0:T(8,128)S(1)} %add.63.mine_ref, f32[16,32,128]{2,1,0:T(8,128)S(1)} %collective-permute-done.30.other_ref, f32[32,64,128]{2,1,0:T(8,128)S(1)} %get-tuple-element.111.prior_ref, ...), custom_call_target="tpu_custom_call" | custom-call | tf_op jit(solution)/shard_map/third/pallas_call | solution.py:505
  142.1 1.8 %collective-permute-start.33 = (f32[64,64]{1,0:T(8,128)S(1)}, f32[64,64]{1,0:T(8,128)S(1)}, u32[]{:S(2)}, u32[]{:S(2)}) collective-permute-start(f32[64,64]{1,0:T(8,128)S(1)} %get-tuple-element.109), channel_id=1, source_target_pairs={{0,4},{4,0},{8,12},{12,8},{1,5},{5,1},{9,13},{13,9},{2,6},{6,2},{1... | collective-permute-start | bytes 49160 | tf_op jit(solution)/shard_map/ppermute | solution.py:131
  143.9 1.9 %collective-permute-done.31 = f32[64,128]{1,0:T(8,128)S(1)} collective-permute-done((f32[64,128]{1,0:T(8,128)S(1)}, f32[64,128]{1,0:T(8,128)S(1)}, u32[]{:S(2)}, u32[]{:S(2)}) %collective-permute-start.31) | collective-permute-done | bytes 32800 | tf_op jit(solution)/shard_map/ppermute | solution.py:131
  146.1 2.7 %collective-permute-start.34 = (f32[64,64]{1,0:T(8,128)S(1)}, f32[64,64]{1,0:T(8,128)S(1)}, u32[]{:S(2)}, u32[]{:S(2)}) collective-permute-start(f32[64,64]{1,0:T(8,128)S(1)} %add.66), channel_id=1, source_target_pairs={{0,8},{4,12},{8,0},{12,4},{1,9},{5,13},{9,1},{13,5},{2,10},{6,14},... | collective-permute-start | bytes 49160 | tf_op jit(solution)/shard_map/ppermute | solution.py:131
  148.8 2.2 %collective-permute-done.34 = f32[64,64]{1,0:T(8,128)S(1)} collective-permute-done((f32[64,64]{1,0:T(8,128)S(1)}, f32[64,64]{1,0:T(8,128)S(1)}, u32[]{:S(2)}, u32[]{:S(2)}) %collective-permute-start.34) | collective-permute-done | bytes 16416 | tf_op jit(solution)/shard_map/ppermute | solution.py:131
  151.0 6.3 %fourth.1 = (f32[64,64]{1,0:T(8,128)S(1)}, f32[64,64]{1,0:T(8,128)S(1)}, f32[64,128]{1,0:T(8,128)S(1)}) custom-call(f32[64,128]{1,0:T(8,128)S(1)} %add.65.gram_ref, f32[64,64]{1,0:T(8,128)S(1)} %add.67.norm_ref), custom_call_target="tpu_custom_call" | custom-call | tf_op jit(solution)/shard_map/fourth/pallas_call | solution.py:514
  157.2 2.3 %last.1 = (f32[32,64,128]{2,1,0:T(8,128)}, f32[4,64,64]{2,1,0:T(8,128)}) custom-call(f32[32,64,128]{2,1,0:T(8,128)S(1)} %get-tuple-element.113.w_ref, f32[32,64,128]{2,1,0:T(8,128)S(1)} %get-tuple-element.112.q_ref, f32[64,128]{1,0:T(8,128)S(1)} %get-tuple-element.115.coef_ref, f32[64,64]{1,0:T(8,128)S(1)} %get-tuple-element.116.a1_ref, ...), custom_call_target="tpu_custom_call" | custom-call | tf_op jit(solution)/shard_map/last/pallas_call | solution.py:517
  (100 shorter events, 36.7 us)
Async XLA Ops:
  0.6 14.7 %collective-permute-start.2 = (s32[1,1,44]{2,1,0:T(1,128)}, s32[1,1,44]{2,1,0:T(1,128)S(1)}, u32[]{:S(2)}, u32[]{:S(2)}) collective-permute-start(s32[1,1,44]{2,1,0:T(1,128)} %cols_ref.3), channel_id=1, source_target_pairs={{4,8},{0,12},{8,4},{12,0},{5,9},{1,13},{9,5},{13,1},{6,10},{2,14},... | collective-permute-start | bytes 536 | tf_op jit(solution)/shard_map/ppermute | solution.py:113
  5.8 9.6 %collective-permute-start.1 = (s32[1,1,44]{2,1,0:T(1,128)}, s32[1,1,44]{2,1,0:T(1,128)S(1)}, u32[]{:S(2)}, u32[]{:S(2)}) collective-permute-start(s32[1,1,44]{2,1,0:T(1,128)} %cols_ref.3), channel_id=1, source_target_pairs={{0,4},{8,12},{4,0},{12,8},{1,5},{9,13},{5,1},{13,9},{2,6},{10,14},... | collective-permute-start | bytes 536 | tf_op jit(solution)/shard_map/ppermute | solution.py:113
  5.8 9.6 %collective-permute-start = (s32[1,1,44]{2,1,0:T(1,128)}, s32[1,1,44]{2,1,0:T(1,128)S(1)}, u32[]{:S(2)}, u32[]{:S(2)}) collective-permute-start(s32[1,1,44]{2,1,0:T(1,128)} %cols_ref.3), channel_id=1, source_target_pairs={{0,8},{4,12},{8,0},{12,4},{1,9},{5,13},{9,1},{13,5},{2,10},{6,14},... | collective-permute-start | bytes 536 | tf_op jit(solution)/shard_map/ppermute | solution.py:113
  16.9 6.0 %collective-permute-start.10 = (f32[8,32,128]{2,1,0:T(8,128)S(1)}, f32[8,32,128]{2,1,0:T(8,128)S(1)}, u32[]{:S(2)}, u32[]{:S(2)}) collective-permute-start(f32[8,32,128]{2,1,0:T(8,128)S(1)} %get-tuple-element.67), channel_id=1, source_target_pairs={{0,4},{8,12},{4,0},{12,8},{1,5},{9,13},{5,1},{13,9},{2,6},{10,14},... | collective-permute-start | bytes 393224 | tf_op jit(solution)/shard_map/ppermute | solution.py:113
  18.1 9.1 %collective-permute-start.9 = (f32[8,32,128]{2,1,0:T(8,128)S(1)}, f32[8,32,128]{2,1,0:T(8,128)S(1)}, u32[]{:S(2)}, u32[]{:S(2)}) collective-permute-start(f32[8,32,128]{2,1,0:T(8,128)S(1)} %get-tuple-element.70), channel_id=1, source_target_pairs={{4,8},{0,12},{8,4},{12,0},{5,9},{1,13},{9,5},{13,1},{6,10},{2,14},... | collective-permute-start | bytes 393224 | tf_op jit(solution)/shard_map/ppermute | solution.py:113
  20.2 11.3 %collective-permute-start.8 = (f32[8,32,128]{2,1,0:T(8,128)S(1)}, f32[8,32,128]{2,1,0:T(8,128)S(1)}, u32[]{:S(2)}, u32[]{:S(2)}) collective-permute-start(f32[8,32,128]{2,1,0:T(8,128)S(1)} %get-tuple-element.69), channel_id=1, source_target_pairs={{0,8},{4,12},{8,0},{12,4},{1,9},{5,13},{9,1},{13,5},{2,10},{6,14},... | collective-permute-start | bytes 393224 | tf_op jit(solution)/shard_map/ppermute | solution.py:113
  32.5 7.0 %collective-permute-start.11 = (f32[16,32,128]{2,1,0:T(8,128)S(1)}, f32[16,32,128]{2,1,0:T(8,128)S(1)}, u32[]{:S(2)}, u32[]{:S(2)}) collective-permute-start(f32[16,32,128]{2,1,0:T(8,128)S(1)} %get-tuple-element.75), channel_id=1, source_target_pairs={{0,1},{1,0},{2,3},{3,2},{4,5},{5,4},{6,7},{7,6},{8,9},{9,8},{10,11... | collective-permute-start | bytes 786440 | tf_op jit(solution)/shard_map/ppermute | solution.py:460
  32.5 5.9 %collective-permute-start.5 = (f32[8,32,128]{2,1,0:T(8,128)S(1)}, f32[8,32,128]{2,1,0:T(8,128)S(1)}, u32[]{:S(2)}, u32[]{:S(2)}) collective-permute-start(f32[8,32,128]{2,1,0:T(8,128)S(1)} %get-tuple-element.65), channel_id=1, source_target_pairs={{0,4},{8,12},{4,0},{12,8},{1,5},{9,13},{5,1},{13,9},{2,6},{10,14},... | collective-permute-start | bytes 393224 | tf_op jit(solution)/shard_map/ppermute | solution.py:113
  39.5 20.0 %collective-permute-start.13 = (f32[16,32,128]{2,1,0:T(8,128)S(1)}, f32[16,32,128]{2,1,0:T(8,128)S(1)}, u32[]{:S(2)}, u32[]{:S(2)}) collective-permute-start(f32[16,32,128]{2,1,0:T(8,128)S(1)} %add.54), channel_id=1, source_target_pairs={{0,2},{1,3},{2,0},{3,1},{4,6},{5,7},{6,4},{7,5},{8,10},{9,11},{10,... | collective-permute-start | bytes 786440 | tf_op jit(solution)/shard_map/ppermute | solution.py:416
  41.1 17.4 %collective-permute-start.4 = (f32[8,32,128]{2,1,0:T(8,128)S(1)}, f32[8,32,128]{2,1,0:T(8,128)S(1)}, u32[]{:S(2)}, u32[]{:S(2)}) collective-permute-start(f32[8,32,128]{2,1,0:T(8,128)S(1)} %get-tuple-element.64), channel_id=1, source_target_pairs={{4,8},{0,12},{8,4},{12,0},{5,9},{1,13},{9,5},{13,1},{6,10},{2,14},... | collective-permute-start | bytes 393224 | tf_op jit(solution)/shard_map/ppermute | solution.py:113
  42.8 4.9 %collective-permute-start.6 = (f32[64,64]{1,0:T(8,128)S(1)}, f32[64,64]{1,0:T(8,128)S(1)}, u32[]{:S(2)}, u32[]{:S(2)}) collective-permute-start(f32[64,64]{1,0:T(8,128)S(1)} %gram.1), channel_id=1, source_target_pairs={{0,4},{4,0},{8,12},{12,8},{1,5},{5,1},{9,13},{13,9},{2,6},{6,2},{1... | collective-permute-start | bytes 49160 | tf_op jit(solution)/shard_map/ppermute | solution.py:131
  47.7 5.2 %collective-permute-start.7 = (f32[64,64]{1,0:T(8,128)S(1)}, f32[64,64]{1,0:T(8,128)S(1)}, u32[]{:S(2)}, u32[]{:S(2)}) collective-permute-start(f32[64,64]{1,0:T(8,128)S(1)} %add.52), channel_id=1, source_target_pairs={{0,8},{4,12},{8,0},{12,4},{1,9},{5,13},{9,1},{13,5},{2,10},{6,14},... | collective-permute-start | bytes 49160 | tf_op jit(solution)/shard_map/ppermute | solution.py:131
  59.5 10.7 %collective-permute-start.14 = (f32[16,32,128]{2,1,0:T(8,128)S(1)}, f32[16,32,128]{2,1,0:T(8,128)S(1)}, u32[]{:S(2)}, u32[]{:S(2)}) collective-permute-start(f32[16,32,128]{2,1,0:T(8,128)S(1)} %add.55.refs_3_), channel_id=1, source_target_pairs={{0,1},{1,0},{2,3},{3,2},{4,5},{5,4},{6,7},{7,6},{8,9},{9,8},{10,11... | collective-permute-start | bytes 786440 | tf_op jit(solution)/shard_map/ppermute | solution.py:466
  59.6 9.4 %collective-permute-start.3 = (f32[8,32,128]{2,1,0:T(8,128)S(1)}, f32[8,32,128]{2,1,0:T(8,128)S(1)}, u32[]{:S(2)}, u32[]{:S(2)}) collective-permute-start(f32[8,32,128]{2,1,0:T(8,128)S(1)} %get-tuple-element.63), channel_id=1, source_target_pairs={{0,8},{4,12},{8,0},{12,4},{1,9},{5,13},{9,1},{13,5},{2,10},{6,14},... | collective-permute-start | bytes 393224 | tf_op jit(solution)/shard_map/ppermute | solution.py:113
  70.0 8.5 %collective-permute-start.12 = (f32[16,32,128]{2,1,0:T(8,128)S(1)}, f32[16,32,128]{2,1,0:T(8,128)S(1)}, u32[]{:S(2)}, u32[]{:S(2)}) collective-permute-start(f32[16,32,128]{2,1,0:T(8,128)S(1)} %get-tuple-element.80), channel_id=1, source_target_pairs={{0,1},{1,0},{2,3},{3,2},{4,5},{5,4},{6,7},{7,6},{8,9},{9,8},{10,11... | collective-permute-start | bytes 786440 | tf_op jit(solution)/shard_map/ppermute | solution.py:470
  71.6 5.9 %collective-permute-start.15 = (f32[8,32,128]{2,1,0:T(8,128)S(1)}, f32[8,32,128]{2,1,0:T(8,128)S(1)}, u32[]{:S(2)}, u32[]{:S(2)}) collective-permute-start(f32[8,32,128]{2,1,0:T(8,128)S(1)} %get-tuple-element.83), channel_id=1, source_target_pairs={{0,4},{8,12},{4,0},{12,8},{1,5},{9,13},{5,1},{13,9},{2,6},{10,14},... | collective-permute-start | bytes 393224 | tf_op jit(solution)/shard_map/ppermute | solution.py:113
  78.5 8.3 %collective-permute-start.16 = (f32[16,32,128]{2,1,0:T(8,128)S(1)}, f32[16,32,128]{2,1,0:T(8,128)S(1)}, u32[]{:S(2)}, u32[]{:S(2)}) collective-permute-start(f32[16,32,128]{2,1,0:T(8,128)S(1)} %add.56), channel_id=1, source_target_pairs={{0,2},{1,3},{2,0},{3,1},{4,6},{5,7},{6,4},{7,5},{8,10},{9,11},{10,... | collective-permute-start | bytes 786440 | tf_op jit(solution)/shard_map/ppermute | solution.py:416
  79.0 6.8 %collective-permute-start.17 = (f32[8,32,128]{2,1,0:T(8,128)S(1)}, f32[8,32,128]{2,1,0:T(8,128)S(1)}, u32[]{:S(2)}, u32[]{:S(2)}) collective-permute-start(f32[8,32,128]{2,1,0:T(8,128)S(1)} %get-tuple-element.86), channel_id=1, source_target_pairs={{4,8},{0,12},{8,4},{12,0},{5,9},{1,13},{9,5},{13,1},{6,10},{2,14},... | collective-permute-start | bytes 393224 | tf_op jit(solution)/shard_map/ppermute | solution.py:113
  86.9 10.8 %collective-permute-start.18 = (f32[16,32,128]{2,1,0:T(8,128)S(1)}, f32[16,32,128]{2,1,0:T(8,128)S(1)}, u32[]{:S(2)}, u32[]{:S(2)}) collective-permute-start(f32[16,32,128]{2,1,0:T(8,128)S(1)} %add.57.refs_3_), channel_id=1, source_target_pairs={{0,1},{1,0},{2,3},{3,2},{4,5},{5,4},{6,7},{7,6},{8,9},{9,8},{10,11... | collective-permute-start | bytes 786440 | tf_op jit(solution)/shard_map/ppermute | solution.py:476
  87.0 9.6 %collective-permute-start.19 = (f32[8,32,128]{2,1,0:T(8,128)S(1)}, f32[8,32,128]{2,1,0:T(8,128)S(1)}, u32[]{:S(2)}, u32[]{:S(2)}) collective-permute-start(f32[8,32,128]{2,1,0:T(8,128)S(1)} %get-tuple-element.90), channel_id=1, source_target_pairs={{0,8},{4,12},{8,0},{12,4},{1,9},{5,13},{9,1},{13,5},{2,10},{6,14},... | collective-permute-start | bytes 393224 | tf_op jit(solution)/shard_map/ppermute | solution.py:113
  97.6 19.7 %collective-permute-start.25 = (f32[16,32,128]{2,1,0:T(8,128)S(1)}, f32[16,32,128]{2,1,0:T(8,128)S(1)}, u32[]{:S(2)}, u32[]{:S(2)}) collective-permute-start(f32[16,32,128]{2,1,0:T(8,128)S(1)} %get-tuple-element.99), channel_id=1, source_target_pairs={{0,1},{1,0},{2,3},{3,2},{4,5},{5,4},{6,7},{7,6},{8,9},{9,8},{10,11... | collective-permute-start | bytes 786440 | tf_op jit(solution)/shard_map/ppermute | solution.py:481
  99.3 17.0 %collective-permute-start.22 = (f32[8,32,128]{2,1,0:T(8,128)S(1)}, f32[8,32,128]{2,1,0:T(8,128)S(1)}, u32[]{:S(2)}, u32[]{:S(2)}) collective-permute-start(f32[8,32,128]{2,1,0:T(8,128)S(1)} %get-tuple-element.95), channel_id=1, source_target_pairs={{0,4},{8,12},{4,0},{12,8},{1,5},{9,13},{5,1},{13,9},{2,6},{10,14},... | collective-permute-start | bytes 393224 | tf_op jit(solution)/shard_map/ppermute | solution.py:113
  99.4 26.1 %collective-permute-start.21 = (f32[8,32,128]{2,1,0:T(8,128)S(1)}, f32[8,32,128]{2,1,0:T(8,128)S(1)}, u32[]{:S(2)}, u32[]{:S(2)}) collective-permute-start(f32[8,32,128]{2,1,0:T(8,128)S(1)} %get-tuple-element.94), channel_id=1, source_target_pairs={{4,8},{0,12},{8,4},{12,0},{5,9},{1,13},{9,5},{13,1},{6,10},{2,14},... | collective-permute-start | bytes 393224 | tf_op jit(solution)/shard_map/ppermute | solution.py:113
  99.6 26.8 %collective-permute-start.20 = (f32[8,32,128]{2,1,0:T(8,128)S(1)}, f32[8,32,128]{2,1,0:T(8,128)S(1)}, u32[]{:S(2)}, u32[]{:S(2)}) collective-permute-start(f32[8,32,128]{2,1,0:T(8,128)S(1)} %get-tuple-element.93), channel_id=1, source_target_pairs={{0,8},{4,12},{8,0},{12,4},{1,9},{5,13},{9,1},{13,5},{2,10},{6,14},... | collective-permute-start | bytes 393224 | tf_op jit(solution)/shard_map/ppermute | solution.py:113
  103.9 5.5 %collective-permute-start.23 = (f32[64,128]{1,0:T(8,128)S(1)}, f32[64,128]{1,0:T(8,128)S(1)}, u32[]{:S(2)}, u32[]{:S(2)}) collective-permute-start(f32[64,128]{1,0:T(8,128)S(1)} %cross.1), channel_id=1, source_target_pairs={{0,4},{4,0},{8,12},{12,8},{1,5},{5,1},{9,13},{13,9},{2,6},{6,2},{1... | collective-permute-start | bytes 98312 | tf_op jit(solution)/shard_map/ppermute | solution.py:131
  109.4 6.8 %collective-permute-start.24 = (f32[64,128]{1,0:T(8,128)S(1)}, f32[64,128]{1,0:T(8,128)S(1)}, u32[]{:S(2)}, u32[]{:S(2)}) collective-permute-start(f32[64,128]{1,0:T(8,128)S(1)} %add.58), channel_id=1, source_target_pairs={{0,8},{4,12},{8,0},{12,4},{1,9},{5,13},{9,1},{13,5},{2,10},{6,14},... | collective-permute-start | bytes 98312 | tf_op jit(solution)/shard_map/ppermute | solution.py:131
  117.3 10.2 %collective-permute-start.28 = (f32[16,32,128]{2,1,0:T(8,128)S(1)}, f32[16,32,128]{2,1,0:T(8,128)S(1)}, u32[]{:S(2)}, u32[]{:S(2)}) collective-permute-start(f32[16,32,128]{2,1,0:T(8,128)S(1)} %add.60), channel_id=1, source_target_pairs={{0,2},{1,3},{2,0},{3,1},{4,6},{5,7},{6,4},{7,5},{8,10},{9,11},{10,... | collective-permute-start | bytes 786440 | tf_op jit(solution)/shard_map/ppermute | solution.py:416
  129.1 8.4 %collective-permute-start.27 = (f32[16,32,128]{2,1,0:T(8,128)S(1)}, f32[16,32,128]{2,1,0:T(8,128)S(1)}, u32[]{:S(2)}, u32[]{:S(2)}) collective-permute-start(f32[16,32,128]{2,1,0:T(8,128)S(1)} %add.61), channel_id=1, source_target_pairs={{0,2},{1,3},{2,0},{3,1},{4,6},{5,7},{6,4},{7,5},{8,10},{9,11},{10,... | collective-permute-start | bytes 786440 | tf_op jit(solution)/shard_map/ppermute | solution.py:416
  141.8 4.0 %collective-permute-start.31 = (f32[64,128]{1,0:T(8,128)S(1)}, f32[64,128]{1,0:T(8,128)S(1)}, u32[]{:S(2)}, u32[]{:S(2)}) collective-permute-start(f32[64,128]{1,0:T(8,128)S(1)} %get-tuple-element.114), channel_id=1, source_target_pairs={{0,4},{4,0},{8,12},{12,8},{1,5},{5,1},{9,13},{13,9},{2,6},{6,2},{1... | collective-permute-start | bytes 98312 | tf_op jit(solution)/shard_map/ppermute | solution.py:131
  142.1 4.1 %collective-permute-start.33 = (f32[64,64]{1,0:T(8,128)S(1)}, f32[64,64]{1,0:T(8,128)S(1)}, u32[]{:S(2)}, u32[]{:S(2)}) collective-permute-start(f32[64,64]{1,0:T(8,128)S(1)} %get-tuple-element.109), channel_id=1, source_target_pairs={{0,4},{4,0},{8,12},{12,8},{1,5},{5,1},{9,13},{13,9},{2,6},{6,2},{1... | collective-permute-start | bytes 49160 | tf_op jit(solution)/shard_map/ppermute | solution.py:131
  145.8 5.2 %collective-permute-start.32 = (f32[64,128]{1,0:T(8,128)S(1)}, f32[64,128]{1,0:T(8,128)S(1)}, u32[]{:S(2)}, u32[]{:S(2)}) collective-permute-start(f32[64,128]{1,0:T(8,128)S(1)} %add.64), channel_id=1, source_target_pairs={{0,8},{4,12},{8,0},{12,4},{1,9},{5,13},{9,1},{13,5},{2,10},{6,14},... | collective-permute-start | bytes 98312 | tf_op jit(solution)/shard_map/ppermute | solution.py:131
  146.1 4.8 %collective-permute-start.34 = (f32[64,64]{1,0:T(8,128)S(1)}, f32[64,64]{1,0:T(8,128)S(1)}, u32[]{:S(2)}, u32[]{:S(2)}) collective-permute-start(f32[64,64]{1,0:T(8,128)S(1)} %add.66), channel_id=1, source_target_pairs={{0,8},{4,12},{8,0},{12,4},{1,9},{5,13},{9,1},{13,5},{2,10},{6,14},... | collective-permute-start | bytes 49160 | tf_op jit(solution)/shard_map/ppermute | solution.py:131
  (12 other events, 69.5 us)

commit v3 on v2

--- a/solution.py
+++ b/solution.py
@@ -70,7 +70,7 @@
     )
 
 
-def call(body, outs, in_specs, scratch=(), name=None, aliases=None):
+def call(body, outs, in_specs, scratch=(), name=None, aliases=None, weight=0):
     shapes = [
         o if isinstance(o, jax.ShapeDtypeStruct) else jax.ShapeDtypeStruct(o, F32) for o in outs
     ]
@@ -82,6 +82,7 @@
         scratch_shapes=list(scratch),
         compiler_params=pltpu.CompilerParams(vmem_limit_bytes=40 << 20),
         input_output_aliases=aliases or {},
+        cost_estimate=pl.CostEstimate(flops=weight, bytes_accessed=weight, transcendentals=0) if weight else None,
         name=name,
     )
 
@@ -122,15 +123,31 @@
     return jnp.array(table, jnp.int32)
 
 
-def all_sum(block, axis):
+def sum_steps(size):
+    return [1 << n for n in range(size.bit_length() - 1)]
+
+
+def start_sum(block, axis):
+    size = lax.axis_size(axis)
+    if size & (size - 1):
+        return block
+    for step in sum_steps(size)[:-1]:
+        block = block + lax.ppermute(block, axis, [(i, i ^ step) for i in range(size)])
+    return block
+
+
+def end_sum(block, axis, *tokens):
     size = lax.axis_size(axis)
     if size & (size - 1):
         return lax.psum(block, axis)
-    step = 1
-    while step < size:
-        block = block + lax.ppermute(block, axis, [(i, i ^ step) for i in range(size)])
-        step *= 2
+    for step in sum_steps(size)[-1:]:
+        got = lax.ppermute(block, axis, [(i, i ^ step) for i in range(size)])
+        block = block + (after(got, *tokens) if tokens else got)
     return block
+
+
+def all_sum(block, axis, *tokens):
+    return end_sum(start_sum(block, axis), axis, *tokens)
 
 
 def factor(gram):
@@ -310,6 +327,7 @@
             [SMEM] * (3 + size) + [VMEM] * (size + 2),
             [pltpu.VMEM(chunk, F32)] if last else [],
             name="join",
+            weight=10**10,
             aliases=None if last else {3 + 2 * size + 1: 0},
         )(
             place, tile_rows, slot_counts, *[asked[p] for p in members], *[got[p] for p in members], split, acc
@@ -450,27 +468,33 @@
         send_body, [packet] * (2 * count), [SMEM] * (3 + count) + [VMEM] * 2, name="send"
     )(place, tile_rows, slot_counts, *asked, x, split)
     got_a = spread(sent[:count])
-    got_b = spread(sent[count:])
-    (gram,) = call(gram_body, [square], [VMEM], name="gram")(after(x, sent[0]))
-    start_gram = all_sum(gram, "res")
+    sent_b = list(sent[count:])
     for n in range(2):
-        acc_a = join(after(acc_a, gram), got_a, groups[n])
+        acc_a = join(acc_a, got_a, groups[n])
+        acc_a, *gated = lax.optimization_barrier((acc_a, *[sent_b[p] for p in groups[n]]))
+        for p, value in zip(groups[n], gated):
+            sent_b[p] = value
     keep_a, give_a = join(acc_a, got_a, groups[2], last=True)
+    for p in groups[2]:
+        sent_b[p] = after(sent_b[p], keep_a)
+    got_b = spread(sent_b)
+    (gram,) = call(gram_body, [square], [VMEM], name="gram")(after(x, keep_a))
 
     core = lax.ppermute(give_a, "vec", swap)
-    acc_b = join(acc_b, got_b, groups[0])
+    acc_b = join(after(acc_b, gram), got_b, groups[0])
     mine_a = keep_a + after(core, acc_b)
-    (start_inv,) = call(first_body, [square], [VMEM], name="first")(after(start_gram, mine_a))
-    acc_b = join(after(acc_b, start_inv), got_b, groups[1])
+    acc_b = join(acc_b, got_b, groups[1])
     mine_a = across(mine_a, acc_b)
     other_a = lax.ppermute(mine_a, "vec", swap)
     keep_b, give_b = join(acc_b, got_b, groups[2], last=True)
-    y_a, acc_a, got_a = resend(mine_a, after(other_a, keep_b))
+    start_gram = start_sum(gram, "res")
+    y_a, acc_a, got_a = resend(mine_a, after(other_a, keep_b, start_gram))
 
     core = lax.ppermute(give_b, "vec", swap)
     acc_a = join(acc_a, got_a, groups[0])
     mine_b = keep_b + after(core, acc_a)
-    acc_a = own(after(acc_a, mine_b), y_a)
+    (start_inv,) = call(first_body, [square], [VMEM], name="first")(end_sum(start_gram, "res", mine_b))
+    acc_a = own(after(acc_a, start_inv), y_a)
     acc_a = join(acc_a, got_a, groups[1])
     mine_b = across(mine_b, acc_a)
     other_b = lax.ppermute(mine_b, "vec", swap)
@@ -482,10 +506,10 @@
     acc_b = own(after(acc_b, gram), y_b)
     acc_b = join(acc_b, got_b, groups[0])
     mine_a = keep_a + after(core, acc_b)
-    cross_gram = all_sum(gram, "res")
+    cross_gram = all_sum(gram, "res", mine_a)
     cross1, lower1, coef, gain = call(
         second_body, [square, square, (2 * width, 3 * width), square], [VMEM] * 2, name="second"
-    )(after(cross_gram, mine_a), start_inv)
+    )(cross_gram, start_inv)
     acc_b = join(after(acc_b, gain), got_b, groups[1])
     mine_a = across(mine_a, acc_b)
     other_a = lax.ppermute(mine_a, "vec", swap)

time: 160 us -> 137 us (0.86)
  waiting for transfers between devices: 68.7 us -> 34.9 us
  starting transfers between devices: 30.3 us -> 41.5 us
    ppermute x15, waiting for transfers between devices: 43.1 us -> 11.2 us  [exchange(): lax.ppermute(block, axis, [(a, b) for a, b in pairs] + [(b, a) for a, b i...]
    ppermute x15, starting transfers between devices: 16.1 us -> 27 us  [exchange(): lax.ppermute(block, axis, [(a, b) for a, b in pairs] + [(b, a) for a, b i...]
    ppermute x8, waiting for transfers between devices: 21 us -> 17.7 us  [the longest x4 15.5 us: end_sum(): got = lax.ppermute(block, axis, [(i, i ^ step) for i in range(size)])]
    ppermute x4, starting transfers between devices: 4.25 us -> 6.25 us  [across(): got = lax.ppermute(mine, 'vec', [(i, i ^ step) for i in range(lanes)])]
  transfers between devices with their start and end apart: 35 -> 35, of which waited for: 18 -> 15; matrix products, arithmetic and copies ran while one was open for 1% -> 1% of each run, Pallas kernels for 25% -> 27%
where the time goes in v3:
time: 137 us
  Pallas kernels  53.2 us (39%)
  starting transfers between devices  41.5 us (30%)
  waiting for transfers between devices  34.9 us (25%)
  local copies, waits for them, and re-layouts  5.77 us (4%)
    ppermute x15, starting transfers between devices, exchange(): lax.ppermute(block, axis, [(a, b) for a, b in pairs] + [(b, a) for a, b i...  27 us
    ppermute x4, waiting for transfers between devices, end_sum(): got = lax.ppermute(block, axis, [(i, i ^ step) for i in range(size)])  15.5 us
    pallas_call x12, Pallas kernels, join(): call(body, [halfchunk] * 2 if last else [chunk], [SMEM] * (3 + size) + [V...  11.7 us
    ppermute x15, waiting for transfers between devices, exchange(): lax.ppermute(block, axis, [(a, b) for a, b in pairs] + [(b, a) for a, b i...  11.2 us
    pallas_call x1, Pallas kernels, local(): call(second_body, [square, square, (2 * width, 3 * width), square], [VMEM...  6.47 us
    pallas_call x1, Pallas kernels, local(): call(fourth_body, [square, square, (width, 2 * width)], [VMEM] * 2, name=...  6.25 us
    ppermute x4, starting transfers between devices, across(): got = lax.ppermute(mine, 'vec', [(i, i ^ step) for i in range(lanes)])  6.25 us
    pallas_call x1, Pallas kernels, local(): call(blend_body, [full, full, square], [SMEM] + [VMEM] * 6, [pltpu.VMEM(c...  5.71 us
  transfers between devices with their start and end apart: 35, of which 15 were waited for; matrix products, arithmetic and copies ran while one was open for 1% of the time, Pallas kernels for 27%

profile of v3, /device:TPU:0, one launch (start us, length us, event | category | flops | bytes accessed | tf_op | source)
XLA Modules:
  0.0 136.9 jit_solution(244166149754143640)
XLA Ops:
  0.6 4.1 %collective-permute-start = (s32[1,1,44]{2,1,0:T(1,128)}, s32[1,1,44]{2,1,0:T(1,128)S(1)}, u32[]{:S(2)}, u32[]{:S(2)}) collective-permute-start(s32[1,1,44]{2,1,0:T(1,128)} %cols_ref.3), channel_id=1, source_target_pairs={{0,8},{4,12},{8,0},{12,4},{1,9},{5,13},{9,1},{13,5},{2,10},{6,14},... | collective-permute-start | bytes 536 | tf_op jit(solution)/shard_map/ppermute | solution.py:114
  4.7 1.6 %collective-permute-start.1 = (s32[1,1,44]{2,1,0:T(1,128)}, s32[1,1,44]{2,1,0:T(1,128)S(1)}, u32[]{:S(2)}, u32[]{:S(2)}) collective-permute-start(s32[1,1,44]{2,1,0:T(1,128)} %cols_ref.3), channel_id=1, source_target_pairs={{0,4},{8,12},{4,0},{12,8},{1,5},{9,13},{5,1},{13,9},{2,6},{10,14},... | collective-permute-start | bytes 536 | tf_op jit(solution)/shard_map/ppermute | solution.py:114
  7.1 1.8 %copy-done = f32[1,1,44,128,128]{4,3,2,1,0:T(8,128)S(1)} copy-done((f32[1,1,44,128,128]{4,3,2,1,0:T(8,128)S(1)}, f32[1,1,44,128,128]{4,3,2,1,0:T(8,128)}, u32[]{:S(2)}) %copy-start) | copy-done | bytes 2883608
  12.2 3.1 %prepare.1 = (f32[32,64,128]{2,1,0:T(8,128)S(1)}, bf16[44,2,128,128]{3,2,1,0:T(8,128)(2,1)S(1)}, f32[32,32,128]{2,1,0:T(8,128)S(1)}, f32[32,32,128]{2,1,0:T(8,128)S(1)}) custom-call(s32[1,1,44]{2,1,0:T(1,128)S(1)} %copy-done.4, s32[1,1,44]{2,1,0:T(1,128)S(1)} %copy-done.6, f32[32,64,128]{2,1,0:T(8,128)S(1)} %copy-done.1, f32[32,128]{1,0:T(8,128)S(1)} %copy-done.2, ...), custom_call_target="tpu_custom_call" | custom-call | tf_op jit(solution)/shard_map/prepare/pallas_call | solution.py:454
  17.5 3.0 %collective-permute-start.3 = (f32[8,32,128]{2,1,0:T(8,128)S(1)}, f32[8,32,128]{2,1,0:T(8,128)S(1)}, u32[]{:S(2)}, u32[]{:S(2)}) collective-permute-start(f32[8,32,128]{2,1,0:T(8,128)S(1)} %get-tuple-element.67), channel_id=1, source_target_pairs={{0,8},{4,12},{8,0},{12,4},{1,9},{5,13},{9,1},{13,5},{2,10},{6,14},... | collective-permute-start | bytes 393224 | tf_op jit(solution)/shard_map/ppermute | solution.py:114
  21.2 2.0 %collective-permute-done.5.refs_1_ = f32[8,32,128]{2,1,0:T(8,128)S(1)} collective-permute-done((f32[8,32,128]{2,1,0:T(8,128)S(1)}, f32[8,32,128]{2,1,0:T(8,128)S(1)}, u32[]{:S(2)}, u32[]{:S(2)}) %collective-permute-start.5) | collective-permute-done | bytes 131104 | tf_op jit(solution)/shard_map/ppermute | solution.py:114
  24.2 4.0 %collective-permute-done.4.refs_1_ = f32[8,32,128]{2,1,0:T(8,128)S(1)} collective-permute-done((f32[8,32,128]{2,1,0:T(8,128)S(1)}, f32[8,32,128]{2,1,0:T(8,128)S(1)}, u32[]{:S(2)}, u32[]{:S(2)}) %collective-permute-start.4) | collective-permute-done | bytes 131104 | tf_op jit(solution)/shard_map/ppermute | solution.py:114
  29.1 3.7 %collective-permute-start.8 = (f32[8,32,128]{2,1,0:T(8,128)S(1)}, f32[8,32,128]{2,1,0:T(8,128)S(1)}, u32[]{:S(2)}, u32[]{:S(2)}) collective-permute-start(f32[8,32,128]{2,1,0:T(8,128)S(1)} %get-tuple-element.78), channel_id=1, source_target_pairs={{0,4},{8,12},{4,0},{12,8},{1,5},{9,13},{5,1},{13,9},{2,6},{10,14},... | collective-permute-start | bytes 393224 | tf_op jit(solution)/shard_map/ppermute | solution.py:114
  34.6 2.2 %collective-permute-start.6 = (f32[8,32,128]{2,1,0:T(8,128)S(1)}, f32[8,32,128]{2,1,0:T(8,128)S(1)}, u32[]{:S(2)}, u32[]{:S(2)}) collective-permute-start(f32[8,32,128]{2,1,0:T(8,128)S(1)} %get-tuple-element.76), channel_id=1, source_target_pairs={{0,8},{4,12},{8,0},{12,4},{1,9},{5,13},{9,1},{13,5},{2,10},{6,14},... | collective-permute-start | bytes 393224 | tf_op jit(solution)/shard_map/ppermute | solution.py:114
  36.8 2.1 %collective-permute-start.7 = (f32[8,32,128]{2,1,0:T(8,128)S(1)}, f32[8,32,128]{2,1,0:T(8,128)S(1)}, u32[]{:S(2)}, u32[]{:S(2)}) collective-permute-start(f32[8,32,128]{2,1,0:T(8,128)S(1)} %get-tuple-element.77), channel_id=1, source_target_pairs={{4,8},{0,12},{8,4},{12,0},{5,9},{1,13},{9,5},{13,1},{6,10},{2,14},... | collective-permute-start | bytes 393224 | tf_op jit(solution)/shard_map/ppermute | solution.py:114
  41.5 4.2 %collective-permute-done.7.refs_1_ = f32[8,32,128]{2,1,0:T(8,128)S(1)} collective-permute-done((f32[8,32,128]{2,1,0:T(8,128)S(1)}, f32[8,32,128]{2,1,0:T(8,128)S(1)}, u32[]{:S(2)}, u32[]{:S(2)}) %collective-permute-start.7) | collective-permute-done | bytes 131104 | tf_op jit(solution)/shard_map/ppermute | solution.py:114
  51.3 3.0 %collective-permute-start.14 = (f32[8,32,128]{2,1,0:T(8,128)S(1)}, f32[8,32,128]{2,1,0:T(8,128)S(1)}, u32[]{:S(2)}, u32[]{:S(2)}) collective-permute-start(f32[8,32,128]{2,1,0:T(8,128)S(1)} %get-tuple-element.88), channel_id=1, source_target_pairs={{0,4},{8,12},{4,0},{12,8},{1,5},{9,13},{5,1},{13,9},{2,6},{10,14},... | collective-permute-start | bytes 393224 | tf_op jit(solution)/shard_map/ppermute | solution.py:114
  54.3 2.4 %collective-permute-start.16 = (f32[8,32,128]{2,1,0:T(8,128)S(1)}, f32[8,32,128]{2,1,0:T(8,128)S(1)}, u32[]{:S(2)}, u32[]{:S(2)}) collective-permute-start(f32[8,32,128]{2,1,0:T(8,128)S(1)} %get-tuple-element.91), channel_id=1, source_target_pairs={{4,8},{0,12},{8,4},{12,0},{5,9},{1,13},{9,5},{13,1},{6,10},{2,14},... | collective-permute-start | bytes 393224 | tf_op jit(solution)/shard_map/ppermute | solution.py:114
  61.0 4.5 %collective-permute-done.17 = f32[64,64]{1,0:T(8,128)S(1)} collective-permute-done((f32[64,64]{1,0:T(8,128)S(1)}, f32[64,64]{1,0:T(8,128)S(1)}, u32[]{:S(2)}, u32[]{:S(2)}) %collective-permute-start.17) | collective-permute-done | bytes 16416 | tf_op jit(solution)/shard_map/ppermute | solution.py:144
  65.5 5.5 %first.1.inverse_ref = f32[64,64]{1,0:T(8,128)S(1)} custom-call(f32[64,64]{1,0:T(8,128)S(1)} %add.56.gram_ref), custom_call_target="tpu_custom_call" | custom-call | tf_op jit(solution)/shard_map/first/pallas_call | solution.py:496
  71.0 1.7 %own.2.refs_3_ = f32[32,32,128]{2,1,0:T(8,128)S(1)} custom-call(s32[1,1,44]{2,1,0:T(1,128)S(1)} %copy-done.5, s32[1,1,44]{2,1,0:T(1,128)S(1)} %copy-done.7, f32[32,32,128]{2,1,0:T(8,128)S(1)} %get-tuple-element.92.x_ref.a_ref, bf16[44,2,128,128]{3,2,1,0:T(8,128)(2,1)S(1)} %get-tuple-element.65.refs_4_.refs_2_.refs_6_.split_ref, ...), custom_call_target="tpu_custom_call", output_to_operand_aliasing={{}: (4, {})} | custom-call | tf_op jit(solution)/shard_map/own/pallas_call | solution.py:449
  75.4 1.6 %resend.3 = (f32[32,32,128]{2,1,0:T(8,128)S(1)}, f32[32,32,128]{2,1,0:T(8,128)S(1)}, f32[8,32,128]{2,1,0:T(8,128)S(1)}, f32[8,32,128]{2,1,0:T(8,128)S(1)}, f32[8,32,128]{2,1,0:T(8,128)S(1)}) custom-call(s32[4]{0:T(128)S(1)} %pad_add_fusion.place_ref, s32[1,1,44]{2,1,0:T(1,128)S(1)} %copy-done.5, s32[1,1,3]{2,1,0:T(1,128)S(1)} %copy-done.8, ...), custom_call_target="tpu_custom_call" | custom-call | tf_op jit(solution)/shard_map/resend/pallas_call | solution.py:440
  78.1 2.1 %collective-permute-start.23 = (f32[64,128]{1,0:T(8,128)S(1)}, f32[64,128]{1,0:T(8,128)S(1)}, u32[]{:S(2)}, u32[]{:S(2)}) collective-permute-start(f32[64,128]{1,0:T(8,128)S(1)} %cross.1), channel_id=1, source_target_pairs={{0,4},{4,0},{8,12},{12,8},{1,5},{5,1},{9,13},{13,9},{2,6},{6,2},{1... | collective-permute-start | bytes 98312 | tf_op jit(solution)/shard_map/ppermute | solution.py:135
  80.2 2.5 %collective-permute-start.21 = (f32[8,32,128]{2,1,0:T(8,128)S(1)}, f32[8,32,128]{2,1,0:T(8,128)S(1)}, u32[]{:S(2)}, u32[]{:S(2)}) collective-permute-start(f32[8,32,128]{2,1,0:T(8,128)S(1)} %get-tuple-element.100), channel_id=1, source_target_pairs={{4,8},{0,12},{8,4},{12,0},{5,9},{1,13},{9,5},{13,1},{6,10},{2,14},... | collective-permute-start | bytes 393224 | tf_op jit(solution)/shard_map/ppermute | solution.py:114
  82.7 1.7 %own.3.refs_3_ = f32[32,32,128]{2,1,0:T(8,128)S(1)} custom-call(s32[1,1,44]{2,1,0:T(1,128)S(1)} %copy-done.5, s32[1,1,44]{2,1,0:T(1,128)S(1)} %copy-done.7, f32[32,32,128]{2,1,0:T(8,128)S(1)} %get-tuple-element.102.b_ref.x_ref, bf16[44,2,128,128]{3,2,1,0:T(8,128)(2,1)S(1)} %get-tuple-element.65.refs_4_.refs_2_.refs_6_.split_ref, ...), custom_call_target="tpu_custom_call", output_to_operand_aliasing={{}: (4, {})} | custom-call | tf_op jit(solution)/shard_map/own/pallas_call | solution.py:449
  86.0 1.6 %collective-permute-start.28 = (f32[16,32,128]{2,1,0:T(8,128)S(1)}, f32[16,32,128]{2,1,0:T(8,128)S(1)}, u32[]{:S(2)}, u32[]{:S(2)}) collective-permute-start(f32[16,32,128]{2,1,0:T(8,128)S(1)} %add.59), channel_id=1, source_target_pairs={{0,2},{1,3},{2,0},{3,1},{4,6},{5,7},{6,4},{7,5},{8,10},{9,11},{10,... | collective-permute-start | bytes 786440 | tf_op jit(solution)/shard_map/ppermute | solution.py:434
  87.6 8.8 %collective-permute-done.24 = f32[64,128]{1,0:T(8,128)S(1)} collective-permute-done((f32[64,128]{1,0:T(8,128)S(1)}, f32[64,128]{1,0:T(8,128)S(1)}, u32[]{:S(2)}, u32[]{:S(2)}) %collective-permute-start.24) | collective-permute-done | bytes 32800 | tf_op jit(solution)/shard_map/ppermute | solution.py:144
  96.4 6.5 %second.1 = (f32[64,64]{1,0:T(8,128)S(1)}, f32[64,64]{1,0:T(8,128)S(1)}, f32[128,192]{1,0:T(8,128)S(1)}, f32[64,64]{1,0:T(8,128)S(1)}) custom-call(f32[64,128]{1,0:T(8,128)S(1)} %add.60.gram_ref, f32[64,64]{1,0:T(8,128)S(1)} %first.1.inverse_ref), custom_call_target="tpu_custom_call" | custom-call | tf_op jit(solution)/shard_map/second/pallas_call | solution.py:510
  106.5 1.6 %collective-permute-start.27 = (f32[16,32,128]{2,1,0:T(8,128)S(1)}, f32[16,32,128]{2,1,0:T(8,128)S(1)}, u32[]{:S(2)}, u32[]{:S(2)}) collective-permute-start(f32[16,32,128]{2,1,0:T(8,128)S(1)} %add.61), channel_id=1, source_target_pairs={{0,2},{1,3},{2,0},{3,1},{4,6},{5,7},{6,4},{7,5},{8,10},{9,11},{10,... | collective-permute-start | bytes 786440 | tf_op jit(solution)/shard_map/ppermute | solution.py:434
  108.1 5.7 %blend.1 = (f32[32,64,128]{2,1,0:T(8,128)S(1)}, f32[32,64,128]{2,1,0:T(8,128)S(1)}, f32[64,64]{1,0:T(8,128)S(1)}) custom-call(s32[4]{0:T(128)S(1)} %pad_add_fusion.place_ref, f32[32,64,128]{2,1,0:T(8,128)S(1)} %get-tuple-element.80.refs_3_.x_ref, f32[32,32,128]{2,1,0:T(8,128)S(1)} %get-tuple-element.92.x_ref.a_ref, ...), custom_call_target="tpu_custom_call" | custom-call | tf_op jit(solution)/shard_map/blend/pallas_call | solution.py:520
  116.6 2.6 %third.1 = (f32[32,64,128]{2,1,0:T(8,128)S(1)}, f32[64,128]{1,0:T(8,128)S(1)}) custom-call(s32[4]{0:T(128)S(1)} %pad_add_fusion.place_ref, f32[16,32,128]{2,1,0:T(8,128)S(1)} %add.63.mine_ref, f32[16,32,128]{2,1,0:T(8,128)S(1)} %collective-permute-done.30.other_ref, f32[32,64,128]{2,1,0:T(8,128)S(1)} %get-tuple-element.117.prior_ref, ...), custom_call_target="tpu_custom_call" | custom-call | tf_op jit(solution)/shard_map/third/pallas_call | solution.py:529
  119.3 2.0 %collective-permute-start.33 = (f32[64,64]{1,0:T(8,128)S(1)}, f32[64,64]{1,0:T(8,128)S(1)}, u32[]{:S(2)}, u32[]{:S(2)}) collective-permute-start(f32[64,64]{1,0:T(8,128)S(1)} %get-tuple-element.115), channel_id=1, source_target_pairs={{0,4},{4,0},{8,12},{12,8},{1,5},{5,1},{9,13},{13,9},{2,6},{6,2},{1... | collective-permute-start | bytes 49160 | tf_op jit(solution)/shard_map/ppermute | solution.py:135
  121.3 1.9 %collective-permute-done.31 = f32[64,128]{1,0:T(8,128)S(1)} collective-permute-done((f32[64,128]{1,0:T(8,128)S(1)}, f32[64,128]{1,0:T(8,128)S(1)}, u32[]{:S(2)}, u32[]{:S(2)}) %collective-permute-start.31) | collective-permute-done | bytes 32800 | tf_op jit(solution)/shard_map/ppermute | solution.py:135
  123.5 2.7 %collective-permute-start.34 = (f32[64,64]{1,0:T(8,128)S(1)}, f32[64,64]{1,0:T(8,128)S(1)}, u32[]{:S(2)}, u32[]{:S(2)}) collective-permute-start(f32[64,64]{1,0:T(8,128)S(1)} %add.66), channel_id=1, source_target_pairs={{0,8},{4,12},{8,0},{12,4},{1,9},{5,13},{9,1},{13,5},{2,10},{6,14},... | collective-permute-start | bytes 49160 | tf_op jit(solution)/shard_map/ppermute | solution.py:144
  126.2 2.2 %collective-permute-done.34 = f32[64,64]{1,0:T(8,128)S(1)} collective-permute-done((f32[64,64]{1,0:T(8,128)S(1)}, f32[64,64]{1,0:T(8,128)S(1)}, u32[]{:S(2)}, u32[]{:S(2)}) %collective-permute-start.34) | collective-permute-done | bytes 16416 | tf_op jit(solution)/shard_map/ppermute | solution.py:144
  128.4 6.3 %fourth.1 = (f32[64,64]{1,0:T(8,128)S(1)}, f32[64,64]{1,0:T(8,128)S(1)}, f32[64,128]{1,0:T(8,128)S(1)}) custom-call(f32[64,128]{1,0:T(8,128)S(1)} %add.65.gram_ref, f32[64,64]{1,0:T(8,128)S(1)} %add.67.norm_ref), custom_call_target="tpu_custom_call" | custom-call | tf_op jit(solution)/shard_map/fourth/pallas_call | solution.py:538
  134.6 2.2 %last.1 = (f32[32,64,128]{2,1,0:T(8,128)}, f32[4,64,64]{2,1,0:T(8,128)}) custom-call(f32[32,64,128]{2,1,0:T(8,128)S(1)} %get-tuple-element.119.w_ref, f32[32,64,128]{2,1,0:T(8,128)S(1)} %get-tuple-element.118.q_ref, f32[64,128]{1,0:T(8,128)S(1)} %get-tuple-element.121.coef_ref, f32[64,64]{1,0:T(8,128)S(1)} %get-tuple-element.122.a1_ref, ...), custom_call_target="tpu_custom_call" | custom-call | tf_op jit(solution)/shard_map/last/pallas_call | solution.py:541
  (100 shorter events, 34.9 us)
Async XLA Ops:
  0.6 14.7 %collective-permute-start = (s32[1,1,44]{2,1,0:T(1,128)}, s32[1,1,44]{2,1,0:T(1,128)S(1)}, u32[]{:S(2)}, u32[]{:S(2)}) collective-permute-start(s32[1,1,44]{2,1,0:T(1,128)} %cols_ref.3), channel_id=1, source_target_pairs={{0,8},{4,12},{8,0},{12,4},{1,9},{5,13},{9,1},{13,5},{2,10},{6,14},... | collective-permute-start | bytes 536 | tf_op jit(solution)/shard_map/ppermute | solution.py:114
  4.7 10.6 %collective-permute-start.1 = (s32[1,1,44]{2,1,0:T(1,128)}, s32[1,1,44]{2,1,0:T(1,128)S(1)}, u32[]{:S(2)}, u32[]{:S(2)}) collective-permute-start(s32[1,1,44]{2,1,0:T(1,128)} %cols_ref.3), channel_id=1, source_target_pairs={{0,4},{8,12},{4,0},{12,8},{1,5},{9,13},{5,1},{13,9},{2,6},{10,14},... | collective-permute-start | bytes 536 | tf_op jit(solution)/shard_map/ppermute | solution.py:114
  6.3 9.0 %collective-permute-start.2 = (s32[1,1,44]{2,1,0:T(1,128)}, s32[1,1,44]{2,1,0:T(1,128)S(1)}, u32[]{:S(2)}, u32[]{:S(2)}) collective-permute-start(s32[1,1,44]{2,1,0:T(1,128)} %cols_ref.3), channel_id=1, source_target_pairs={{4,8},{0,12},{8,4},{12,0},{5,9},{1,13},{9,5},{13,1},{6,10},{2,14},... | collective-permute-start | bytes 536 | tf_op jit(solution)/shard_map/ppermute | solution.py:114
  16.8 6.4 %collective-permute-start.5 = (f32[8,32,128]{2,1,0:T(8,128)S(1)}, f32[8,32,128]{2,1,0:T(8,128)S(1)}, u32[]{:S(2)}, u32[]{:S(2)}) collective-permute-start(f32[8,32,128]{2,1,0:T(8,128)S(1)} %get-tuple-element.69), channel_id=1, source_target_pairs={{0,4},{8,12},{4,0},{12,8},{1,5},{9,13},{5,1},{13,9},{2,6},{10,14},... | collective-permute-start | bytes 393224 | tf_op jit(solution)/shard_map/ppermute | solution.py:114
  17.5 15.4 %collective-permute-start.3 = (f32[8,32,128]{2,1,0:T(8,128)S(1)}, f32[8,32,128]{2,1,0:T(8,128)S(1)}, u32[]{:S(2)}, u32[]{:S(2)}) collective-permute-start(f32[8,32,128]{2,1,0:T(8,128)S(1)} %get-tuple-element.67), channel_id=1, source_target_pairs={{0,8},{4,12},{8,0},{12,4},{1,9},{5,13},{9,1},{13,5},{2,10},{6,14},... | collective-permute-start | bytes 393224 | tf_op jit(solution)/shard_map/ppermute | solution.py:114
  20.5 7.7 %collective-permute-start.4 = (f32[8,32,128]{2,1,0:T(8,128)S(1)}, f32[8,32,128]{2,1,0:T(8,128)S(1)}, u32[]{:S(2)}, u32[]{:S(2)}) collective-permute-start(f32[8,32,128]{2,1,0:T(8,128)S(1)} %get-tuple-element.68), channel_id=1, source_target_pairs={{4,8},{0,12},{8,4},{12,0},{5,9},{1,13},{9,5},{13,1},{6,10},{2,14},... | collective-permute-start | bytes 393224 | tf_op jit(solution)/shard_map/ppermute | solution.py:114
  29.1 9.8 %collective-permute-start.8 = (f32[8,32,128]{2,1,0:T(8,128)S(1)}, f32[8,32,128]{2,1,0:T(8,128)S(1)}, u32[]{:S(2)}, u32[]{:S(2)}) collective-permute-start(f32[8,32,128]{2,1,0:T(8,128)S(1)} %get-tuple-element.78), channel_id=1, source_target_pairs={{0,4},{8,12},{4,0},{12,8},{1,5},{9,13},{5,1},{13,9},{2,6},{10,14},... | collective-permute-start | bytes 393224 | tf_op jit(solution)/shard_map/ppermute | solution.py:114
  34.4 4.5 %collective-permute-start.13 = (f32[64,64]{1,0:T(8,128)S(1)}, f32[64,64]{1,0:T(8,128)S(1)}, u32[]{:S(2)}, u32[]{:S(2)}) collective-permute-start(f32[64,64]{1,0:T(8,128)S(1)} %gram.1), channel_id=1, source_target_pairs={{0,4},{4,0},{8,12},{12,8},{1,5},{5,1},{9,13},{13,9},{2,6},{6,2},{1... | collective-permute-start | bytes 49160 | tf_op jit(solution)/shard_map/ppermute | solution.py:135
  34.5 5.4 %collective-permute-start.10 = (f32[16,32,128]{2,1,0:T(8,128)S(1)}, f32[16,32,128]{2,1,0:T(8,128)S(1)}, u32[]{:S(2)}, u32[]{:S(2)}) collective-permute-start(f32[16,32,128]{2,1,0:T(8,128)S(1)} %get-tuple-element.84), channel_id=1, source_target_pairs={{0,1},{1,0},{2,3},{3,2},{4,5},{5,4},{6,7},{7,6},{8,9},{9,8},{10,11... | collective-permute-start | bytes 786440 | tf_op jit(solution)/shard_map/ppermute | solution.py:483
  34.6 13.7 %collective-permute-start.6 = (f32[8,32,128]{2,1,0:T(8,128)S(1)}, f32[8,32,128]{2,1,0:T(8,128)S(1)}, u32[]{:S(2)}, u32[]{:S(2)}) collective-permute-start(f32[8,32,128]{2,1,0:T(8,128)S(1)} %get-tuple-element.76), channel_id=1, source_target_pairs={{0,8},{4,12},{8,0},{12,4},{1,9},{5,13},{9,1},{13,5},{2,10},{6,14},... | collective-permute-start | bytes 393224 | tf_op jit(solution)/shard_map/ppermute | solution.py:114
  36.8 8.9 %collective-permute-start.7 = (f32[8,32,128]{2,1,0:T(8,128)S(1)}, f32[8,32,128]{2,1,0:T(8,128)S(1)}, u32[]{:S(2)}, u32[]{:S(2)}) collective-permute-start(f32[8,32,128]{2,1,0:T(8,128)S(1)} %get-tuple-element.77), channel_id=1, source_target_pairs={{4,8},{0,12},{8,4},{12,0},{5,9},{1,13},{9,5},{13,1},{6,10},{2,14},... | collective-permute-start | bytes 393224 | tf_op jit(solution)/shard_map/ppermute | solution.py:114
  39.9 8.2 %collective-permute-start.11 = (f32[16,32,128]{2,1,0:T(8,128)S(1)}, f32[16,32,128]{2,1,0:T(8,128)S(1)}, u32[]{:S(2)}, u32[]{:S(2)}) collective-permute-start(f32[16,32,128]{2,1,0:T(8,128)S(1)} %add.52), channel_id=1, source_target_pairs={{0,2},{1,3},{2,0},{3,1},{4,6},{5,7},{6,4},{7,5},{8,10},{9,11},{10,... | collective-permute-start | bytes 786440 | tf_op jit(solution)/shard_map/ppermute | solution.py:434
  48.2 1.6 %collective-permute-start.12 = (f32[16,32,128]{2,1,0:T(8,128)S(1)}, f32[16,32,128]{2,1,0:T(8,128)S(1)}, u32[]{:S(2)}, u32[]{:S(2)}) collective-permute-start(f32[16,32,128]{2,1,0:T(8,128)S(1)} %add.53.refs_3_), channel_id=1, source_target_pairs={{0,1},{1,0},{2,3},{3,2},{4,5},{5,4},{6,7},{7,6},{8,9},{9,8},{10,11... | collective-permute-start | bytes 786440 | tf_op jit(solution)/shard_map/ppermute | solution.py:488
  51.3 7.2 %collective-permute-start.14 = (f32[8,32,128]{2,1,0:T(8,128)S(1)}, f32[8,32,128]{2,1,0:T(8,128)S(1)}, u32[]{:S(2)}, u32[]{:S(2)}) collective-permute-start(f32[8,32,128]{2,1,0:T(8,128)S(1)} %get-tuple-element.88), channel_id=1, source_target_pairs={{0,4},{8,12},{4,0},{12,8},{1,5},{9,13},{5,1},{13,9},{2,6},{10,14},... | collective-permute-start | bytes 393224 | tf_op jit(solution)/shard_map/ppermute | solution.py:114
  54.3 11.2 %collective-permute-start.17 = (f32[64,64]{1,0:T(8,128)S(1)}, f32[64,64]{1,0:T(8,128)S(1)}, u32[]{:S(2)}, u32[]{:S(2)}) collective-permute-start(f32[64,64]{1,0:T(8,128)S(1)} %add.54), channel_id=1, source_target_pairs={{0,8},{4,12},{8,0},{12,4},{1,9},{5,13},{9,1},{13,5},{2,10},{6,14},... | collective-permute-start | bytes 49160 | tf_op jit(solution)/shard_map/ppermute | solution.py:144
  54.3 5.1 %collective-permute-start.9 = (f32[16,32,128]{2,1,0:T(8,128)S(1)}, f32[16,32,128]{2,1,0:T(8,128)S(1)}, u32[]{:S(2)}, u32[]{:S(2)}) collective-permute-start(f32[16,32,128]{2,1,0:T(8,128)S(1)} %get-tuple-element.83), channel_id=1, source_target_pairs={{0,1},{1,0},{2,3},{3,2},{4,5},{5,4},{6,7},{7,6},{8,9},{9,8},{10,11... | collective-permute-start | bytes 786440 | tf_op jit(solution)/shard_map/ppermute | solution.py:493
  54.3 18.5 %collective-permute-start.16 = (f32[8,32,128]{2,1,0:T(8,128)S(1)}, f32[8,32,128]{2,1,0:T(8,128)S(1)}, u32[]{:S(2)}, u32[]{:S(2)}) collective-permute-start(f32[8,32,128]{2,1,0:T(8,128)S(1)} %get-tuple-element.91), channel_id=1, source_target_pairs={{4,8},{0,12},{8,4},{12,0},{5,9},{1,13},{9,5},{13,1},{6,10},{2,14},... | collective-permute-start | bytes 393224 | tf_op jit(solution)/shard_map/ppermute | solution.py:114
  56.8 17.1 %collective-permute-start.19 = (f32[8,32,128]{2,1,0:T(8,128)S(1)}, f32[8,32,128]{2,1,0:T(8,128)S(1)}, u32[]{:S(2)}, u32[]{:S(2)}) collective-permute-start(f32[8,32,128]{2,1,0:T(8,128)S(1)} %get-tuple-element.96), channel_id=1, source_target_pairs={{0,8},{4,12},{8,0},{12,4},{1,9},{5,13},{9,1},{13,5},{2,10},{6,14},... | collective-permute-start | bytes 393224 | tf_op jit(solution)/shard_map/ppermute | solution.py:114
  59.5 14.3 %collective-permute-start.15 = (f32[16,32,128]{2,1,0:T(8,128)S(1)}, f32[16,32,128]{2,1,0:T(8,128)S(1)}, u32[]{:S(2)}, u32[]{:S(2)}) collective-permute-start(f32[16,32,128]{2,1,0:T(8,128)S(1)} %add.55), channel_id=1, source_target_pairs={{0,2},{1,3},{2,0},{3,1},{4,6},{5,7},{6,4},{7,5},{8,10},{9,11},{10,... | collective-permute-start | bytes 786440 | tf_op jit(solution)/shard_map/ppermute | solution.py:434
  77.0 7.9 %collective-permute-start.22 = (f32[8,32,128]{2,1,0:T(8,128)S(1)}, f32[8,32,128]{2,1,0:T(8,128)S(1)}, u32[]{:S(2)}, u32[]{:S(2)}) collective-permute-start(f32[8,32,128]{2,1,0:T(8,128)S(1)} %get-tuple-element.101), channel_id=1, source_target_pairs={{0,4},{8,12},{4,0},{12,8},{1,5},{9,13},{5,1},{13,9},{2,6},{10,14},... | collective-permute-start | bytes 393224 | tf_op jit(solution)/shard_map/ppermute | solution.py:114
  78.1 6.3 %collective-permute-start.23 = (f32[64,128]{1,0:T(8,128)S(1)}, f32[64,128]{1,0:T(8,128)S(1)}, u32[]{:S(2)}, u32[]{:S(2)}) collective-permute-start(f32[64,128]{1,0:T(8,128)S(1)} %cross.1), channel_id=1, source_target_pairs={{0,4},{4,0},{8,12},{12,8},{1,5},{5,1},{9,13},{13,9},{2,6},{6,2},{1... | collective-permute-start | bytes 98312 | tf_op jit(solution)/shard_map/ppermute | solution.py:135
  80.2 5.7 %collective-permute-start.25 = (f32[16,32,128]{2,1,0:T(8,128)S(1)}, f32[16,32,128]{2,1,0:T(8,128)S(1)}, u32[]{:S(2)}, u32[]{:S(2)}) collective-permute-start(f32[16,32,128]{2,1,0:T(8,128)S(1)} %get-tuple-element.105), channel_id=1, source_target_pairs={{0,1},{1,0},{2,3},{3,2},{4,5},{5,4},{6,7},{7,6},{8,9},{9,8},{10,11... | collective-permute-start | bytes 786440 | tf_op jit(solution)/shard_map/ppermute | solution.py:505
  80.2 23.6 %collective-permute-start.20 = (f32[8,32,128]{2,1,0:T(8,128)S(1)}, f32[8,32,128]{2,1,0:T(8,128)S(1)}, u32[]{:S(2)}, u32[]{:S(2)}) collective-permute-start(f32[8,32,128]{2,1,0:T(8,128)S(1)} %get-tuple-element.99), channel_id=1, source_target_pairs={{0,8},{4,12},{8,0},{12,4},{1,9},{5,13},{9,1},{13,5},{2,10},{6,14},... | collective-permute-start | bytes 393224 | tf_op jit(solution)/shard_map/ppermute | solution.py:114
  80.2 22.6 %collective-permute-start.21 = (f32[8,32,128]{2,1,0:T(8,128)S(1)}, f32[8,32,128]{2,1,0:T(8,128)S(1)}, u32[]{:S(2)}, u32[]{:S(2)}) collective-permute-start(f32[8,32,128]{2,1,0:T(8,128)S(1)} %get-tuple-element.100), channel_id=1, source_target_pairs={{4,8},{0,12},{8,4},{12,0},{5,9},{1,13},{9,5},{13,1},{6,10},{2,14},... | collective-permute-start | bytes 393224 | tf_op jit(solution)/shard_map/ppermute | solution.py:114
  84.5 11.9 %collective-permute-start.24 = (f32[64,128]{1,0:T(8,128)S(1)}, f32[64,128]{1,0:T(8,128)S(1)}, u32[]{:S(2)}, u32[]{:S(2)}) collective-permute-start(f32[64,128]{1,0:T(8,128)S(1)} %add.58), channel_id=1, source_target_pairs={{0,8},{4,12},{8,0},{12,4},{1,9},{5,13},{9,1},{13,5},{2,10},{6,14},... | collective-permute-start | bytes 98312 | tf_op jit(solution)/shard_map/ppermute | solution.py:144
  86.0 19.0 %collective-permute-start.28 = (f32[16,32,128]{2,1,0:T(8,128)S(1)}, f32[16,32,128]{2,1,0:T(8,128)S(1)}, u32[]{:S(2)}, u32[]{:S(2)}) collective-permute-start(f32[16,32,128]{2,1,0:T(8,128)S(1)} %add.59), channel_id=1, source_target_pairs={{0,2},{1,3},{2,0},{3,1},{4,6},{5,7},{6,4},{7,5},{8,10},{9,11},{10,... | collective-permute-start | bytes 786440 | tf_op jit(solution)/shard_map/ppermute | solution.py:434
  105.1 3.0 %collective-permute-start.29 = (f32[16,32,128]{2,1,0:T(8,128)S(1)}, f32[16,32,128]{2,1,0:T(8,128)S(1)}, u32[]{:S(2)}, u32[]{:S(2)}) collective-permute-start(f32[16,32,128]{2,1,0:T(8,128)S(1)} %add.62.mine_ref), channel_id=1, source_target_pairs={{0,1},{1,0},{2,3},{3,2},{4,5},{5,4},{6,7},{7,6},{8,9},{9,8},{10,11... | collective-permute-start | bytes 786440 | tf_op jit(solution)/shard_map/ppermute | solution.py:515
  106.5 8.4 %collective-permute-start.27 = (f32[16,32,128]{2,1,0:T(8,128)S(1)}, f32[16,32,128]{2,1,0:T(8,128)S(1)}, u32[]{:S(2)}, u32[]{:S(2)}) collective-permute-start(f32[16,32,128]{2,1,0:T(8,128)S(1)} %add.61), channel_id=1, source_target_pairs={{0,2},{1,3},{2,0},{3,1},{4,6},{5,7},{6,4},{7,5},{8,10},{9,11},{10,... | collective-permute-start | bytes 786440 | tf_op jit(solution)/shard_map/ppermute | solution.py:434
  119.2 4.0 %collective-permute-start.31 = (f32[64,128]{1,0:T(8,128)S(1)}, f32[64,128]{1,0:T(8,128)S(1)}, u32[]{:S(2)}, u32[]{:S(2)}) collective-permute-start(f32[64,128]{1,0:T(8,128)S(1)} %get-tuple-element.120), channel_id=1, source_target_pairs={{0,4},{4,0},{8,12},{12,8},{1,5},{5,1},{9,13},{13,9},{2,6},{6,2},{1... | collective-permute-start | bytes 98312 | tf_op jit(solution)/shard_map/ppermute | solution.py:135
  119.3 4.3 %collective-permute-start.33 = (f32[64,64]{1,0:T(8,128)S(1)}, f32[64,64]{1,0:T(8,128)S(1)}, u32[]{:S(2)}, u32[]{:S(2)}) collective-permute-start(f32[64,64]{1,0:T(8,128)S(1)} %get-tuple-element.115), channel_id=1, source_target_pairs={{0,4},{4,0},{8,12},{12,8},{1,5},{5,1},{9,13},{13,9},{2,6},{6,2},{1... | collective-permute-start | bytes 49160 | tf_op jit(solution)/shard_map/ppermute | solution.py:135
  123.2 5.2 %collective-permute-start.32 = (f32[64,128]{1,0:T(8,128)S(1)}, f32[64,128]{1,0:T(8,128)S(1)}, u32[]{:S(2)}, u32[]{:S(2)}) collective-permute-start(f32[64,128]{1,0:T(8,128)S(1)} %add.64), channel_id=1, source_target_pairs={{0,8},{4,12},{8,0},{12,4},{1,9},{5,13},{9,1},{13,5},{2,10},{6,14},... | collective-permute-start | bytes 98312 | tf_op jit(solution)/shard_map/ppermute | solution.py:144
  123.5 4.8 %collective-permute-start.34 = (f32[64,64]{1,0:T(8,128)S(1)}, f32[64,64]{1,0:T(8,128)S(1)}, u32[]{:S(2)}, u32[]{:S(2)}) collective-permute-start(f32[64,64]{1,0:T(8,128)S(1)} %add.66), channel_id=1, source_target_pairs={{0,8},{4,12},{8,0},{12,4},{1,9},{5,13},{9,1},{13,5},{2,10},{6,14},... | collective-permute-start | bytes 49160 | tf_op jit(solution)/shard_map/ppermute | solution.py:144
  (12 other events, 51.3 us)

commit v4 on v3

--- a/solution.py
+++ b/solution.py
@@ -85,6 +85,10 @@
         cost_estimate=pl.CostEstimate(flops=weight, bytes_accessed=weight, transcendentals=0) if weight else None,
         name=name,
     )
+
+
+def pinned(value):
+    return pltpu.with_memory_space_constraint(value, pltpu.HBM)
 
 
 def after(value, *tokens):
@@ -152,21 +156,45 @@
 
 def factor(gram):
     size = gram.shape[0]
+    tile = (8, 2 * size)
     row_id = lax.broadcasted_iota(jnp.int32, (size, size), 0)
     col_id = lax.broadcasted_iota(jnp.int32, (size, size), 1)
     work = jnp.concatenate([gram, (row_id == col_id).astype(F32)], axis=1)
     blocks = [work[8 * b : 8 * b + 8] for b in range(size // 8)]
-    sub = lax.broadcasted_iota(jnp.int32, (8, 2 * size), 0)
-    for j in range(size):
+    sub = lax.broadcasted_iota(jnp.int32, tile, 0)
+    for j in range(0, size, 4):
         b, s = divmod(j, 8)
-        row = blocks[b][s : s + 1]
-        scaled = row / row[:, j : j + 1]
-        scaled = jnp.broadcast_to(scaled, (8, 2 * size))
-        for other in range(b, size // 8):
-            col = jnp.broadcast_to(blocks[other][:, j : j + 1], (8, 2 * size))
-            if other == b:
-                col = jnp.where(sub > s, col, 0.0)
-            blocks[other] = blocks[other] - col * scaled
+        later = range(b + s // 4, size // 8)
+        line = [jnp.broadcast_to(blocks[b][s + k : s + k + 1], tile) for k in range(4)]
+        cols = {
+            o: [jnp.broadcast_to(blocks[o][:, j + k : j + k + 1], tile) for k in range(4)]
+            for o in range(b, size // 8)
+        }
+        entry = {
+            (k, l): jnp.broadcast_to(cols[b][l][s + k : s + k + 1], tile)
+            for k in range(4)
+            for l in range(k, 4)
+        }
+        scaled = []
+        for k in range(4):
+            inverse = 1.0 / entry[k, k]
+            for l in range(k + 1, 4):
+                ratio = entry[k, l] * inverse
+                for p in range(l, 4):
+                    entry[l, p] = entry[l, p] - ratio * entry[k, p]
+                line[l] = line[l] - ratio * line[k]
+                for o in later:
+                    cols[o][l] = cols[o][l] - ratio * cols[o][k]
+            scaled.append(inverse * line[k])
+        for o in range(b, size // 8):
+            new = blocks[o]
+            if o in later:
+                new = new - ((cols[o][0] * scaled[0] + cols[o][1] * scaled[1]) + (cols[o][2] * scaled[2] + cols[o][3] * scaled[3]))
+            if o == b:
+                new = jnp.where(sub > s + 3, new, blocks[o])
+                for k in range(1, 4):
+                    new = jnp.where(sub == s + k, line[k], new)
+            blocks[o] = new
     work = jnp.concatenate(blocks, axis=0)
     pivots = jnp.sum(jnp.where(row_id == col_id, work[:, :size], 0.0), axis=1, keepdims=True)
     work = work / jnp.sqrt(pivots)
@@ -185,6 +213,7 @@
     rounds = pairings(peers)
     count = len(rounds)
     full = (rows, width, length)
+    halffull = (half, width, length)
     chunk = (rows, part, length)
     halfchunk = (half, part, length)
     packet = (CAP, part, length)
@@ -373,39 +402,53 @@
         coef_ref[width:, width : 2 * width] = gain
         coef_ref[width:, 2 * width :] = jnp.zeros(square, F32)
 
-    def blend_body(place_ref, x_ref, a_ref, b_ref, mine_ref, other_ref, coef_ref, w_ref, q_ref, out_ref, z_ref):
-        settle(place_ref, mine_ref, other_ref, z_ref)
-        total = jnp.zeros(square, F32)
-        for n in range(0, rows, 2):
-            qs = []
-            stacks = [
-                jnp.concatenate([x_ref[m], a_ref[m], b_ref[m], z_ref[m]], axis=0) for m in (n, n + 1)
-            ]
-            for m, both in zip((n, n + 1), wide_product(coef_ref[:, : 2 * width + part], stacks)):
-                w_ref[m] = both[:width]
-                q_ref[m] = both[width:]
-                qs.append(both[width:])
-            total += gram_step(qs, [qs])
-        out_ref[...] = total
-
-    def third_body(place_ref, mine_ref, other_ref, prior_ref, q_ref, gain_ref, w_ref, out_ref, z_ref):
+    def blend(side, mine, other, coef):
+        def body(place_ref, x_ref, a_ref, b_ref, mine_ref, other_ref, coef_ref, w_ref, q_ref, out_ref, z_ref):
+            settle(place_ref, mine_ref, other_ref, z_ref)
+            total = jnp.zeros(square, F32)
+            for n in range(0, half, 2):
+                qs = []
+                stacks = [
+                    jnp.concatenate([ref[side * half + m] for ref in (x_ref, a_ref, b_ref, z_ref)], axis=0)
+                    for m in (n, n + 1)
+                ]
+                for m, both in zip((n, n + 1), wide_product(coef_ref[:, : 2 * width + part], stacks)):
+                    w_ref[m] = both[:width]
+                    q_ref[m] = both[width:]
+                    qs.append(both[width:])
+                total += gram_step(qs, [qs])
+            out_ref[...] = total
+
+        return call(
+            body,
+            [halffull, halffull, square],
+            [SMEM] + [VMEM] * 6,
+            [pltpu.VMEM(chunk, F32)],
+            name="blend",
+        )(place, x, y_a, y_b, mine, other, coef)
+
+    def third_body(place_ref, mine_ref, other_ref, gain_ref, *refs):
+        prior_refs, q_refs, norm_refs = refs[0:2], refs[2:4], refs[4:6]
+        w_ref, out_ref, z_ref = refs[6:]
         settle(place_ref, mine_ref, other_ref, z_ref)
         total = jnp.zeros((width, 2 * width), F32)
         for n in range(0, rows, 2):
+            side, m = divmod(n, half)
             ws = []
-            for m, w in zip((n, n + 1), wide_product(gain_ref[:, part:], [z_ref[n], z_ref[n + 1]])):
-                w = w + prior_ref[m]
-                w_ref[m] = w
+            for k, w in enumerate(wide_product(gain_ref[:, part:], [z_ref[n], z_ref[n + 1]])):
+                w = w + prior_refs[side][m + k]
+                w_ref[n + k] = w
                 ws.append(w)
-            total += gram_step(ws, [[q_ref[n], q_ref[n + 1]], ws])
-        out_ref[...] = total
-
-    def fourth_body(gram_ref, norm_ref, cross_ref, lower_ref, coef_ref):
+            total += gram_step(ws, [[q_refs[side][m], q_refs[side][m + 1]], ws])
+        out_ref[:, : 2 * width] = total
+        out_ref[:, 2 * width :] = norm_refs[0][...] + norm_refs[1][...]
+
+    def fourth_body(gram_ref, cross_ref, lower_ref, coef_ref):
         cross = gram_ref[:, :width]
-        norm = norm_ref[...]
+        norm = gram_ref[:, 2 * width :]
         taken = cross + SHIFT * (norm - identity())
         mixed = dot(taken, cross, tb=True)
-        squared = gram_ref[:, width:] - mixed - mixed.T + dot(dot(taken, norm), taken, tb=True)
+        squared = gram_ref[:, width : 2 * width] - mixed - mixed.T + dot(dot(taken, norm), taken, tb=True)
         upper, inverse = factor(squared)
         cross_ref[...] = taken + SHIFT * identity()
         lower_ref[...] = upper.T
@@ -413,11 +456,13 @@
         coef_ref[:, :width] = inverse * scale
         coef_ref[:, width:] = -dot(inverse, taken) * scale
 
-    def last_body(w_ref, q_ref, coef_ref, a1_ref, l1_ref, a2_ref, l2_ref, out_ref, pack_ref):
+    def last_body(w_ref, low_ref, high_ref, coef_ref, a1_ref, l1_ref, a2_ref, l2_ref, out_ref, pack_ref):
         for n, ref in enumerate((a1_ref, l1_ref, a2_ref, l2_ref)):
             pack_ref[n] = ref[...]
         for n in range(0, rows, 2):
-            stacks = [jnp.concatenate([w_ref[m], q_ref[m]], axis=0) for m in (n, n + 1)]
+            side, at = divmod(n, half)
+            q_ref = (low_ref, high_ref)[side]
+            stacks = [jnp.concatenate([w_ref[n + k], q_ref[at + k]], axis=0) for k in range(2)]
             for m, out in zip((n, n + 1), wide_product(coef_ref[...], stacks)):
                 out_ref[m] = out
 
@@ -463,7 +508,7 @@
             pltpu.SemaphoreType.DMA((8,)),
         ],
         name="prepare",
-    )(tile_rows, tile_cols, start_block, diagonal, hess_tiles)
+    )(*[pinned(v) for v in (tile_rows, tile_cols, start_block, diagonal, hess_tiles)])
     sent = call(
         send_body, [packet] * (2 * count), [SMEM] * (3 + count) + [VMEM] * 2, name="send"
     )(place, tile_rows, slot_counts, *asked, x, split)
@@ -471,30 +516,32 @@
     sent_b = list(sent[count:])
     for n in range(2):
         acc_a = join(acc_a, got_a, groups[n])
-        acc_a, *gated = lax.optimization_barrier((acc_a, *[sent_b[p] for p in groups[n]]))
+        acc_a, x, *gated = lax.optimization_barrier((acc_a, x, *[sent_b[p] for p in groups[n]]))
         for p, value in zip(groups[n], gated):
             sent_b[p] = value
+        if n == 0:
+            (gram,) = call(gram_body, [square], [VMEM], name="gram")(x)
+            start_gram = start_sum(gram, "res")
+    acc_a = after(acc_a, start_gram)
     keep_a, give_a = join(acc_a, got_a, groups[2], last=True)
     for p in groups[2]:
         sent_b[p] = after(sent_b[p], keep_a)
     got_b = spread(sent_b)
-    (gram,) = call(gram_body, [square], [VMEM], name="gram")(after(x, keep_a))
 
     core = lax.ppermute(give_a, "vec", swap)
-    acc_b = join(after(acc_b, gram), got_b, groups[0])
+    acc_b = join(acc_b, got_b, groups[0])
     mine_a = keep_a + after(core, acc_b)
-    acc_b = join(acc_b, got_b, groups[1])
+    (start_inv,) = call(first_body, [square], [VMEM], name="first")(end_sum(start_gram, "res", mine_a))
+    acc_b = join(after(acc_b, start_inv), got_b, groups[1])
     mine_a = across(mine_a, acc_b)
     other_a = lax.ppermute(mine_a, "vec", swap)
     keep_b, give_b = join(acc_b, got_b, groups[2], last=True)
-    start_gram = start_sum(gram, "res")
-    y_a, acc_a, got_a = resend(mine_a, after(other_a, keep_b, start_gram))
+    y_a, acc_a, got_a = resend(mine_a, after(other_a, keep_b))
 
     core = lax.ppermute(give_b, "vec", swap)
     acc_a = join(acc_a, got_a, groups[0])
     mine_b = keep_b + after(core, acc_a)
-    (start_inv,) = call(first_body, [square], [VMEM], name="first")(end_sum(start_gram, "res", mine_b))
-    acc_a = own(after(acc_a, start_inv), y_a)
+    acc_a = own(after(acc_a, mine_b), y_a)
     acc_a = join(acc_a, got_a, groups[1])
     mine_b = across(mine_b, acc_a)
     other_b = lax.ppermute(mine_b, "vec", swap)
@@ -506,40 +553,36 @@
     acc_b = own(after(acc_b, gram), y_b)
     acc_b = join(acc_b, got_b, groups[0])
     mine_a = keep_a + after(core, acc_b)
-    cross_gram = all_sum(gram, "res", mine_a)
-    cross1, lower1, coef, gain = call(
-        second_body, [square, square, (2 * width, 3 * width), square], [VMEM] * 2, name="second"
-    )(cross_gram, start_inv)
-    acc_b = join(after(acc_b, gain), got_b, groups[1])
+    cross_gram = start_sum(gram, "res")
+    acc_b = join(after(acc_b, cross_gram, mine_a), got_b, groups[1])
+    cross_gram = end_sum(cross_gram, "res", acc_b)
+    acc_b = after(acc_b, cross_gram)
     mine_a = across(mine_a, acc_b)
     other_a = lax.ppermute(mine_a, "vec", swap)
     keep_b, give_b = join(acc_b, got_b, groups[2], last=True)
 
     core = lax.ppermute(give_b, "vec", swap)
     mine_b = keep_b + core
-    w_prior, q, norm = call(
-        blend_body,
-        [full, full, square],
-        [SMEM] + [VMEM] * 6,
-        [pltpu.VMEM(chunk, F32)],
-        name="blend",
-    )(place, x, y_a, y_b, mine_a, other_a, after(coef, mine_b))
-    mine_b = across(mine_b, norm)
+    cross1, lower1, coef, gain = call(
+        second_body, [square, square, (2 * width, 3 * width), square], [VMEM] * 2, name="second"
+    )(after(cross_gram, mine_b), start_inv)
+    w_low, q_low, norm_low = blend(0, mine_a, other_a, coef)
+    mine_b = across(mine_b, norm_low)
     other_b = lax.ppermute(mine_b, "vec", swap)
+    w_high, q_high, norm_high = blend(1, mine_a, other_a, after(coef, mine_b))
     w, gram = call(
         third_body,
-        [full, (width, 2 * width)],
-        [SMEM] + [VMEM] * 5,
+        [full, (width, 3 * width)],
+        [SMEM] + [VMEM] * 9,
         [pltpu.VMEM(chunk, F32)],
         name="third",
-    )(place, mine_b, other_b, w_prior, q, gain)
-    norm = all_sum(norm, "res")
+    )(place, mine_b, after(other_b, norm_high), gain, w_low, w_high, q_low, q_high, norm_low, norm_high)
     gram = all_sum(gram, "res")
     cross2, lower2, coef = call(
-        fourth_body, [square, square, (width, 2 * width)], [VMEM] * 2, name="fourth"
-    )(gram, norm)
-    return call(last_body, [full, (4, width, width)], [VMEM] * 7, name="last")(
-        w, q, coef, cross1, lower1, cross2, lower2
+        fourth_body, [square, square, (width, 2 * width)], [VMEM], name="fourth"
+    )(gram)
+    return call(last_body, [full, (4, width, width)], [VMEM] * 8, name="last")(
+        w, q_low, q_high, coef, cross1, lower1, cross2, lower2
     )
 
 

time: 137 us -> 119 us (0.87)
  starting transfers between devices: 41.5 us -> 34.6 us
  Pallas kernels: 53.2 us -> 47 us
  local copies, waits for them, and re-layouts: 5.77 us -> 0.71 us
    unnamed x18 -> x8, local copies, waits for them, and re-layouts: 5.08 us -> 0.02 us
    ppermute x15, starting transfers between devices: 27 us -> 23 us  [exchange(): lax.ppermute(block, axis, [(a, b) for a, b in pairs] + [(b, a) for a, b i...]
    pallas_call x1, Pallas kernels: 6.47 us -> 3.94 us  [local(): call(second_body, [square, square, (2 * width, 3 * width), square], [VMEM...]
    pallas_call x1, Pallas kernels: 5.53 us -> 3 us  [local(): call(first_body, [square], [VMEM], name='first')]
    ppermute x4 -> x3, starting transfers between devices: 3.13 us -> 0.88 us  [end_sum(): got = lax.ppermute(block, axis, [(i, i ^ step) for i in range(size)])]
    ppermute x15, waiting for transfers between devices: 11.2 us -> 13.4 us  [exchange(): lax.ppermute(block, axis, [(a, b) for a, b in pairs] + [(b, a) for a, b i...]
    pallas_call x5 -> x6, Pallas kernels: 17.3 us -> 15.6 us  [the longest x2 6.5 us: blend(): call(body, [halffull, halffull, square], [SMEM] + [VMEM] * 6, [pltpu.VMEM...]
    ppermute x2, waiting for transfers between devices: 2.01 us -> 0.49 us  [local(): other_b = lax.ppermute(mine_b, 'vec', swap)]
  transfers between devices with their start and end apart: 35 -> 33, of which waited for: 15 -> 15; matrix products, arithmetic and copies ran while one was open for 1% -> 1% of each run, Pallas kernels for 27% -> 28%
where the time goes in v4:
time: 119 us
  Pallas kernels  47 us (39%)
  waiting for transfers between devices  35.3 us (30%)
  starting transfers between devices  34.6 us (29%)
    ppermute x15, starting transfers between devices, exchange(): lax.ppermute(block, axis, [(a, b) for a, b in pairs] + [(b, a) for a, b i...  23 us
    ppermute x3, waiting for transfers between devices, end_sum(): got = lax.ppermute(block, axis, [(i, i ^ step) for i in range(size)])  13.9 us
    ppermute x15, waiting for transfers between devices, exchange(): lax.ppermute(block, axis, [(a, b) for a, b in pairs] + [(b, a) for a, b i...  13.4 us
    pallas_call x12, Pallas kernels, join(): call(body, [halfchunk] * 2 if last else [chunk], [SMEM] * (3 + size) + [V...  11.7 us
    pallas_call x2, Pallas kernels, blend(): call(body, [halffull, halffull, square], [SMEM] + [VMEM] * 6, [pltpu.VMEM...  6.5 us
    ppermute x4, starting transfers between devices, across(): got = lax.ppermute(mine, 'vec', [(i, i ^ step) for i in range(lanes)])  6.25 us
    pallas_call x1, Pallas kernels, local(): call(second_body, [square, square, (2 * width, 3 * width), square], [VMEM...  3.94 us
    pallas_call x1, Pallas kernels, local(): call(fourth_body, [square, square, (width, 2 * width)], [VMEM], name='fou...  3.76 us
  transfers between devices with their start and end apart: 33, of which 15 were waited for; matrix products, arithmetic and copies ran while one was open for 1% of the time, Pallas kernels for 28%

profile of v4, /device:TPU:0, one launch (start us, length us, event | category | flops | bytes accessed | tf_op | source)
XLA Modules:
  0.0 119.0 jit_solution(4866430707891972890)
XLA Ops:
  0.7 4.1 %collective-permute-start = (s32[1,1,44]{2,1,0:T(1,128)}, s32[1,1,44]{2,1,0:T(1,128)S(1)}, u32[]{:S(2)}, u32[]{:S(2)}) collective-permute-start(s32[1,1,44]{2,1,0:T(1,128)} %cols_ref.3), channel_id=1, source_target_pairs={{0,8},{4,12},{8,0},{12,4},{1,9},{5,13},{9,1},{13,5},{2,10},{6,14},... | collective-permute-start | bytes 536 | tf_op jit(solution)/shard_map/ppermute | solution.py:118
  4.8 1.6 %collective-permute-start.1 = (s32[1,1,44]{2,1,0:T(1,128)}, s32[1,1,44]{2,1,0:T(1,128)S(1)}, u32[]{:S(2)}, u32[]{:S(2)}) collective-permute-start(s32[1,1,44]{2,1,0:T(1,128)} %cols_ref.3), channel_id=1, source_target_pairs={{0,4},{8,12},{4,0},{12,8},{1,5},{9,13},{5,1},{13,9},{2,6},{10,14},... | collective-permute-start | bytes 536 | tf_op jit(solution)/shard_map/ppermute | solution.py:118
  7.1 3.8 %prepare.1 = (f32[32,64,128]{2,1,0:T(8,128)S(1)}, bf16[44,2,128,128]{3,2,1,0:T(8,128)(2,1)S(1)}, f32[32,32,128]{2,1,0:T(8,128)S(1)}, f32[32,32,128]{2,1,0:T(8,128)S(1)}) custom-call(s32[1,1,44]{2,1,0:T(1,128)} %rows_ref.33, s32[1,1,44]{2,1,0:T(1,128)} %cols_ref.3, f32[32,64,128]{2,1,0:T(8,128)} %x_hbm.1, f32[32,128]{1,0:T(8,128)} %refs_5_.3, ...), custom_call_target="tpu_custom_call" | custom-call | tf_op jit(solution)/shard_map/prepare/pallas_call | solution.py:499
  13.3 2.7 %collective-permute-start.3 = (f32[8,32,128]{2,1,0:T(8,128)S(1)}, f32[8,32,128]{2,1,0:T(8,128)S(1)}, u32[]{:S(2)}, u32[]{:S(2)}) collective-permute-start(f32[8,32,128]{2,1,0:T(8,128)S(1)} %get-tuple-element.75), channel_id=1, source_target_pairs={{0,8},{4,12},{8,0},{12,4},{1,9},{5,13},{9,1},{13,5},{2,10},{6,14},... | collective-permute-start | bytes 393224 | tf_op jit(solution)/shard_map/ppermute | solution.py:118
  16.0 1.7 %collective-permute-start.4 = (f32[8,32,128]{2,1,0:T(8,128)S(1)}, f32[8,32,128]{2,1,0:T(8,128)S(1)}, u32[]{:S(2)}, u32[]{:S(2)}) collective-permute-start(f32[8,32,128]{2,1,0:T(8,128)S(1)} %get-tuple-element.76), channel_id=1, source_target_pairs={{4,8},{0,12},{8,4},{12,0},{5,9},{1,13},{9,5},{13,1},{6,10},{2,14},... | collective-permute-start | bytes 393224 | tf_op jit(solution)/shard_map/ppermute | solution.py:118
  20.5 3.6 %collective-permute-done.4.refs_1_ = f32[8,32,128]{2,1,0:T(8,128)S(1)} collective-permute-done((f32[8,32,128]{2,1,0:T(8,128)S(1)}, f32[8,32,128]{2,1,0:T(8,128)S(1)}, u32[]{:S(2)}, u32[]{:S(2)}) %collective-permute-start.4) | collective-permute-done | bytes 131104 | tf_op jit(solution)/shard_map/ppermute | solution.py:118
  25.1 1.7 %collective-permute-start.8 = (f32[8,32,128]{2,1,0:T(8,128)S(1)}, f32[8,32,128]{2,1,0:T(8,128)S(1)}, u32[]{:S(2)}, u32[]{:S(2)}) collective-permute-start(f32[8,32,128]{2,1,0:T(8,128)S(1)} %get-tuple-element.87), channel_id=1, source_target_pairs={{4,8},{0,12},{8,4},{12,0},{5,9},{1,13},{9,5},{13,1},{6,10},{2,14},... | collective-permute-start | bytes 393224 | tf_op jit(solution)/shard_map/ppermute | solution.py:118
  26.8 2.9 %collective-permute-start.9 = (f32[8,32,128]{2,1,0:T(8,128)S(1)}, f32[8,32,128]{2,1,0:T(8,128)S(1)}, u32[]{:S(2)}, u32[]{:S(2)}) collective-permute-start(f32[8,32,128]{2,1,0:T(8,128)S(1)} %get-tuple-element.88), channel_id=1, source_target_pairs={{0,4},{8,12},{4,0},{12,8},{1,5},{9,13},{5,1},{13,9},{2,6},{10,14},... | collective-permute-start | bytes 393224 | tf_op jit(solution)/shard_map/ppermute | solution.py:118
  31.0 2.4 %collective-permute-start.7 = (f32[8,32,128]{2,1,0:T(8,128)S(1)}, f32[8,32,128]{2,1,0:T(8,128)S(1)}, u32[]{:S(2)}, u32[]{:S(2)}) collective-permute-start(f32[8,32,128]{2,1,0:T(8,128)S(1)} %get-tuple-element.86), channel_id=1, source_target_pairs={{0,8},{4,12},{8,0},{12,4},{1,9},{5,13},{9,1},{13,5},{2,10},{6,14},... | collective-permute-start | bytes 393224 | tf_op jit(solution)/shard_map/ppermute | solution.py:118
  36.8 2.3 %collective-permute-done.10 = f32[64,64]{1,0:T(8,128)S(1)} collective-permute-done((f32[64,64]{1,0:T(8,128)S(1)}, f32[64,64]{1,0:T(8,128)S(1)}, u32[]{:S(2)}, u32[]{:S(2)}) %collective-permute-start.10) | collective-permute-done | bytes 16416 | tf_op jit(solution)/shard_map/ppermute | solution.py:148
  39.2 3.0 %first.1.inverse_ref = f32[64,64]{1,0:T(8,128)S(1)} custom-call(f32[64,64]{1,0:T(8,128)S(1)} %add.48.gram_ref), custom_call_target="tpu_custom_call" | custom-call | tf_op jit(solution)/shard_map/first/pallas_call | solution.py:534
  48.2 1.9 %collective-permute-start.19 = (f32[8,32,128]{2,1,0:T(8,128)S(1)}, f32[8,32,128]{2,1,0:T(8,128)S(1)}, u32[]{:S(2)}, u32[]{:S(2)}) collective-permute-start(f32[8,32,128]{2,1,0:T(8,128)S(1)} %get-tuple-element.105), channel_id=1, source_target_pairs={{0,8},{4,12},{8,0},{12,4},{1,9},{5,13},{9,1},{13,5},{2,10},{6,14},... | collective-permute-start | bytes 393224 | tf_op jit(solution)/shard_map/ppermute | solution.py:118
  50.1 4.8 %collective-permute-done.15.refs_1_ = f32[8,32,128]{2,1,0:T(8,128)S(1)} collective-permute-done((f32[8,32,128]{2,1,0:T(8,128)S(1)}, f32[8,32,128]{2,1,0:T(8,128)S(1)}, u32[]{:S(2)}, u32[]{:S(2)}) %collective-permute-start.15) | collective-permute-done | bytes 131104 | tf_op jit(solution)/shard_map/ppermute | solution.py:118
  55.8 1.6 %collective-permute-start.16 = (f32[16,32,128]{2,1,0:T(8,128)S(1)}, f32[16,32,128]{2,1,0:T(8,128)S(1)}, u32[]{:S(2)}, u32[]{:S(2)}) collective-permute-start(f32[16,32,128]{2,1,0:T(8,128)S(1)} %add.50), channel_id=1, source_target_pairs={{0,2},{1,3},{2,0},{3,1},{4,6},{5,7},{6,4},{7,5},{8,10},{9,11},{10,... | collective-permute-start | bytes 786440 | tf_op jit(solution)/shard_map/ppermute | solution.py:479
  57.4 1.7 %own.2.refs_3_ = f32[32,32,128]{2,1,0:T(8,128)S(1)} custom-call(s32[1,1,44]{2,1,0:T(1,128)S(1)} %copy-done.1, s32[1,1,44]{2,1,0:T(1,128)S(1)} %copy-done.2, f32[32,32,128]{2,1,0:T(8,128)S(1)} %get-tuple-element.102.x_ref.a_ref, bf16[44,2,128,128]{3,2,1,0:T(8,128)(2,1)S(1)} %get-tuple-element.73.refs_4_.refs_2_.refs_6_.split_ref, ...), custom_call_target="tpu_custom_call", output_to_operand_aliasing={{}: (4, {})} | custom-call | tf_op jit(solution)/shard_map/own/pallas_call | solution.py:494
  60.1 2.2 %collective-permute-done.16 = f32[16,32,128]{2,1,0:T(8,128)S(1)} collective-permute-done((f32[16,32,128]{2,1,0:T(8,128)S(1)}, f32[16,32,128]{2,1,0:T(8,128)S(1)}, u32[]{:S(2)}, u32[]{:S(2)}) %collective-permute-start.16) | collective-permute-done | bytes 262176 | tf_op jit(solution)/shard_map/ppermute | solution.py:479
  63.9 1.6 %resend.3 = (f32[32,32,128]{2,1,0:T(8,128)S(1)}, f32[32,32,128]{2,1,0:T(8,128)S(1)}, f32[8,32,128]{2,1,0:T(8,128)S(1)}, f32[8,32,128]{2,1,0:T(8,128)S(1)}, f32[8,32,128]{2,1,0:T(8,128)S(1)}) custom-call(s32[4]{0:T(128)S(1)} %pad_add_fusion.place_ref, s32[1,1,44]{2,1,0:T(1,128)S(1)} %copy-done.1, s32[1,1,3]{2,1,0:T(1,128)S(1)} %copy-done.3, ...), custom_call_target="tpu_custom_call" | custom-call | tf_op jit(solution)/shard_map/resend/pallas_call | solution.py:485
  66.6 2.1 %collective-permute-start.23 = (f32[64,128]{1,0:T(8,128)S(1)}, f32[64,128]{1,0:T(8,128)S(1)}, u32[]{:S(2)}, u32[]{:S(2)}) collective-permute-start(f32[64,128]{1,0:T(8,128)S(1)} %cross.1), channel_id=1, source_target_pairs={{0,4},{4,0},{8,12},{12,8},{1,5},{5,1},{9,13},{13,9},{2,6},{6,2},{1... | collective-permute-start | bytes 98312 | tf_op jit(solution)/shard_map/ppermute | solution.py:139
  68.7 2.5 %collective-permute-start.21 = (f32[8,32,128]{2,1,0:T(8,128)S(1)}, f32[8,32,128]{2,1,0:T(8,128)S(1)}, u32[]{:S(2)}, u32[]{:S(2)}) collective-permute-start(f32[8,32,128]{2,1,0:T(8,128)S(1)} %get-tuple-element.109), channel_id=1, source_target_pairs={{4,8},{0,12},{8,4},{12,0},{5,9},{1,13},{9,5},{13,1},{6,10},{2,14},... | collective-permute-start | bytes 393224 | tf_op jit(solution)/shard_map/ppermute | solution.py:118
  71.2 1.7 %own.3.refs_3_ = f32[32,32,128]{2,1,0:T(8,128)S(1)} custom-call(s32[1,1,44]{2,1,0:T(1,128)S(1)} %copy-done.1, s32[1,1,44]{2,1,0:T(1,128)S(1)} %copy-done.2, f32[32,32,128]{2,1,0:T(8,128)S(1)} %get-tuple-element.111.b_ref.x_ref, bf16[44,2,128,128]{3,2,1,0:T(8,128)(2,1)S(1)} %get-tuple-element.73.refs_4_.refs_2_.refs_6_.split_ref, ...), custom_call_target="tpu_custom_call", output_to_operand_aliasing={{}: (4, {})} | custom-call | tf_op jit(solution)/shard_map/own/pallas_call | solution.py:494
  74.5 1.6 %collective-permute-start.28 = (f32[16,32,128]{2,1,0:T(8,128)S(1)}, f32[16,32,128]{2,1,0:T(8,128)S(1)}, u32[]{:S(2)}, u32[]{:S(2)}) collective-permute-start(f32[16,32,128]{2,1,0:T(8,128)S(1)} %add.53), channel_id=1, source_target_pairs={{0,2},{1,3},{2,0},{3,1},{4,6},{5,7},{6,4},{7,5},{8,10},{9,11},{10,... | collective-permute-start | bytes 786440 | tf_op jit(solution)/shard_map/ppermute | solution.py:479
  76.0 2.3 %collective-permute-done.21.refs_1_ = f32[8,32,128]{2,1,0:T(8,128)S(1)} collective-permute-done((f32[8,32,128]{2,1,0:T(8,128)S(1)}, f32[8,32,128]{2,1,0:T(8,128)S(1)}, u32[]{:S(2)}, u32[]{:S(2)}) %collective-permute-start.21) | collective-permute-done | bytes 131104 | tf_op jit(solution)/shard_map/ppermute | solution.py:118
  79.3 5.6 %collective-permute-done.25 = f32[64,128]{1,0:T(8,128)S(1)} collective-permute-done((f32[64,128]{1,0:T(8,128)S(1)}, f32[64,128]{1,0:T(8,128)S(1)}, u32[]{:S(2)}, u32[]{:S(2)}) %collective-permute-start.25) | collective-permute-done | bytes 32800 | tf_op jit(solution)/shard_map/ppermute | solution.py:148
  87.6 1.6 %collective-permute-start.27 = (f32[16,32,128]{2,1,0:T(8,128)S(1)}, f32[16,32,128]{2,1,0:T(8,128)S(1)}, u32[]{:S(2)}, u32[]{:S(2)}) collective-permute-start(f32[16,32,128]{2,1,0:T(8,128)S(1)} %add.55), channel_id=1, source_target_pairs={{0,2},{1,3},{2,0},{3,1},{4,6},{5,7},{6,4},{7,5},{8,10},{9,11},{10,... | collective-permute-start | bytes 786440 | tf_op jit(solution)/shard_map/ppermute | solution.py:479
  89.1 3.9 %second.1 = (f32[64,64]{1,0:T(8,128)S(1)}, f32[64,64]{1,0:T(8,128)S(1)}, f32[128,192]{1,0:T(8,128)S(1)}, f32[64,64]{1,0:T(8,128)S(1)}) custom-call(f32[64,128]{1,0:T(8,128)S(1)} %add.54.gram_ref, f32[64,64]{1,0:T(8,128)S(1)} %first.1.inverse_ref), custom_call_target="tpu_custom_call" | custom-call | tf_op jit(solution)/shard_map/second/pallas_call | solution.py:566
  93.1 3.2 %blend.2 = (f32[16,64,128]{2,1,0:T(8,128)S(1)}, f32[16,64,128]{2,1,0:T(8,128)S(1)}, f32[64,64]{1,0:T(8,128)S(1)}) custom-call(s32[4]{0:T(128)S(1)} %pad_add_fusion.place_ref, f32[32,64,128]{2,1,0:T(8,128)S(1)} %get-tuple-element.113.refs_3_.x_ref, f32[32,32,128]{2,1,0:T(8,128)S(1)} %get-tuple-element.102.x_ref.a_ref, ...), custom_call_target="tpu_custom_call" | custom-call | tf_op jit(solution)/shard_map/blend/pallas_call | solution.py:422
  96.5 3.2 %blend.3 = (f32[16,64,128]{2,1,0:T(8,128)S(1)}, f32[16,64,128]{2,1,0:T(8,128)S(1)}, f32[64,64]{1,0:T(8,128)S(1)}) custom-call(s32[4]{0:T(128)S(1)} %pad_add_fusion.place_ref, f32[32,64,128]{2,1,0:T(8,128)S(1)} %get-tuple-element.113.refs_3_.x_ref, f32[32,32,128]{2,1,0:T(8,128)S(1)} %get-tuple-element.102.x_ref.a_ref, ...), custom_call_target="tpu_custom_call" | custom-call | tf_op jit(solution)/shard_map/blend/pallas_call | solution.py:422
  99.7 2.6 %third.1 = (f32[32,64,128]{2,1,0:T(8,128)S(1)}, f32[64,192]{1,0:T(8,128)S(1)}) custom-call(s32[4]{0:T(128)S(1)} %pad_add_fusion.place_ref, f32[16,32,128]{2,1,0:T(8,128)S(1)} %add.57.mine_ref, f32[16,32,128]{2,1,0:T(8,128)S(1)} %collective-permute-done.30.other_ref, f32[64,64]{1,0:T(8,128)S(1)} %get-tuple-element.130.gain_ref, ...), custom_call_target="tpu_custom_call" | custom-call | tf_op jit(solution)/shard_map/third/pallas_call | solution.py:573
  103.3 3.6 %collective-permute-done.31 = f32[64,192]{1,0:T(8,128)S(1)} collective-permute-done((f32[64,192]{1,0:T(8,128)S(1)}, f32[64,192]{1,0:T(8,128)S(1)}, u32[]{:S(2)}, u32[]{:S(2)}) %collective-permute-start.31) | collective-permute-done | bytes 49184 | tf_op jit(solution)/shard_map/ppermute | solution.py:139
  107.0 6.0 %collective-permute-done.32 = f32[64,192]{1,0:T(8,128)S(1)} collective-permute-done((f32[64,192]{1,0:T(8,128)S(1)}, f32[64,192]{1,0:T(8,128)S(1)}, u32[]{:S(2)}, u32[]{:S(2)}) %collective-permute-start.32) | collective-permute-done | bytes 49184 | tf_op jit(solution)/shard_map/ppermute | solution.py:148
  113.0 3.8 %fourth.1 = (f32[64,64]{1,0:T(8,128)S(1)}, f32[64,64]{1,0:T(8,128)S(1)}, f32[64,128]{1,0:T(8,128)S(1)}) custom-call(f32[64,192]{1,0:T(8,128)S(1)} %add.59.gram_ref), custom_call_target="tpu_custom_call" | custom-call | tf_op jit(solution)/shard_map/fourth/pallas_call | solution.py:581
  116.8 2.3 %last.1 = (f32[32,64,128]{2,1,0:T(8,128)}, f32[4,64,64]{2,1,0:T(8,128)}) custom-call(f32[32,64,128]{2,1,0:T(8,128)S(1)} %get-tuple-element.135.w_ref, f32[16,64,128]{2,1,0:T(8,128)S(1)} %get-tuple-element.133.refs_2_.low_ref, f32[16,64,128]{2,1,0:T(8,128)S(1)} %get-tuple-element.134.refs_3_.high_ref, f32[64,128]{1,0:T(8,128)S(1)} %get-tuple-element.137.coef_ref, ...), custom_call_target="tpu_custom_call" | custom-call | tf_op jit(solution)/shard_map/last/pallas_call | solution.py:584
  (85 shorter events, 28.6 us)
Async XLA Ops:
  0.7 10.2 %collective-permute-start = (s32[1,1,44]{2,1,0:T(1,128)}, s32[1,1,44]{2,1,0:T(1,128)S(1)}, u32[]{:S(2)}, u32[]{:S(2)}) collective-permute-start(s32[1,1,44]{2,1,0:T(1,128)} %cols_ref.3), channel_id=1, source_target_pairs={{0,8},{4,12},{8,0},{12,4},{1,9},{5,13},{9,1},{13,5},{2,10},{6,14},... | collective-permute-start | bytes 536 | tf_op jit(solution)/shard_map/ppermute | solution.py:118
  4.8 6.1 %collective-permute-start.1 = (s32[1,1,44]{2,1,0:T(1,128)}, s32[1,1,44]{2,1,0:T(1,128)S(1)}, u32[]{:S(2)}, u32[]{:S(2)}) collective-permute-start(s32[1,1,44]{2,1,0:T(1,128)} %cols_ref.3), channel_id=1, source_target_pairs={{0,4},{8,12},{4,0},{12,8},{1,5},{9,13},{5,1},{13,9},{2,6},{10,14},... | collective-permute-start | bytes 536 | tf_op jit(solution)/shard_map/ppermute | solution.py:118
  6.3 5.5 %collective-permute-start.2 = (s32[1,1,44]{2,1,0:T(1,128)}, s32[1,1,44]{2,1,0:T(1,128)S(1)}, u32[]{:S(2)}, u32[]{:S(2)}) collective-permute-start(s32[1,1,44]{2,1,0:T(1,128)} %cols_ref.3), channel_id=1, source_target_pairs={{4,8},{0,12},{8,4},{12,0},{5,9},{1,13},{9,5},{13,1},{6,10},{2,14},... | collective-permute-start | bytes 536 | tf_op jit(solution)/shard_map/ppermute | solution.py:118
  13.3 5.4 %collective-permute-start.5 = (f32[8,32,128]{2,1,0:T(8,128)S(1)}, f32[8,32,128]{2,1,0:T(8,128)S(1)}, u32[]{:S(2)}, u32[]{:S(2)}) collective-permute-start(f32[8,32,128]{2,1,0:T(8,128)S(1)} %get-tuple-element.77), channel_id=1, source_target_pairs={{0,4},{8,12},{4,0},{12,8},{1,5},{9,13},{5,1},{13,9},{2,6},{10,14},... | collective-permute-start | bytes 393224 | tf_op jit(solution)/shard_map/ppermute | solution.py:118
  13.3 16.7 %collective-permute-start.3 = (f32[8,32,128]{2,1,0:T(8,128)S(1)}, f32[8,32,128]{2,1,0:T(8,128)S(1)}, u32[]{:S(2)}, u32[]{:S(2)}) collective-permute-start(f32[8,32,128]{2,1,0:T(8,128)S(1)} %get-tuple-element.75), channel_id=1, source_target_pairs={{0,8},{4,12},{8,0},{12,4},{1,9},{5,13},{9,1},{13,5},{2,10},{6,14},... | collective-permute-start | bytes 393224 | tf_op jit(solution)/shard_map/ppermute | solution.py:118
  16.0 8.1 %collective-permute-start.4 = (f32[8,32,128]{2,1,0:T(8,128)S(1)}, f32[8,32,128]{2,1,0:T(8,128)S(1)}, u32[]{:S(2)}, u32[]{:S(2)}) collective-permute-start(f32[8,32,128]{2,1,0:T(8,128)S(1)} %get-tuple-element.76), channel_id=1, source_target_pairs={{4,8},{0,12},{8,4},{12,0},{5,9},{1,13},{9,5},{13,1},{6,10},{2,14},... | collective-permute-start | bytes 393224 | tf_op jit(solution)/shard_map/ppermute | solution.py:118
  20.2 9.5 %collective-permute-start.6 = (f32[64,64]{1,0:T(8,128)S(1)}, f32[64,64]{1,0:T(8,128)S(1)}, u32[]{:S(2)}, u32[]{:S(2)}) collective-permute-start(f32[64,64]{1,0:T(8,128)S(1)} %gram.1), channel_id=1, source_target_pairs={{0,4},{4,0},{8,12},{12,8},{1,5},{5,1},{9,13},{13,9},{2,6},{6,2},{1... | collective-permute-start | bytes 49160 | tf_op jit(solution)/shard_map/ppermute | solution.py:139
  25.1 17.1 %collective-permute-start.8 = (f32[8,32,128]{2,1,0:T(8,128)S(1)}, f32[8,32,128]{2,1,0:T(8,128)S(1)}, u32[]{:S(2)}, u32[]{:S(2)}) collective-permute-start(f32[8,32,128]{2,1,0:T(8,128)S(1)} %get-tuple-element.87), channel_id=1, source_target_pairs={{4,8},{0,12},{8,4},{12,0},{5,9},{1,13},{9,5},{13,1},{6,10},{2,14},... | collective-permute-start | bytes 393224 | tf_op jit(solution)/shard_map/ppermute | solution.py:118
  26.8 7.5 %collective-permute-start.9 = (f32[8,32,128]{2,1,0:T(8,128)S(1)}, f32[8,32,128]{2,1,0:T(8,128)S(1)}, u32[]{:S(2)}, u32[]{:S(2)}) collective-permute-start(f32[8,32,128]{2,1,0:T(8,128)S(1)} %get-tuple-element.88), channel_id=1, source_target_pairs={{0,4},{8,12},{4,0},{12,8},{1,5},{9,13},{5,1},{13,9},{2,6},{10,14},... | collective-permute-start | bytes 393224 | tf_op jit(solution)/shard_map/ppermute | solution.py:118
  29.7 9.5 %collective-permute-start.10 = (f32[64,64]{1,0:T(8,128)S(1)}, f32[64,64]{1,0:T(8,128)S(1)}, u32[]{:S(2)}, u32[]{:S(2)}) collective-permute-start(f32[64,64]{1,0:T(8,128)S(1)} %add.46), channel_id=1, source_target_pairs={{0,8},{4,12},{8,0},{12,4},{1,9},{5,13},{9,1},{13,5},{2,10},{6,14},... | collective-permute-start | bytes 49160 | tf_op jit(solution)/shard_map/ppermute | solution.py:148
  31.0 12.5 %collective-permute-start.7 = (f32[8,32,128]{2,1,0:T(8,128)S(1)}, f32[8,32,128]{2,1,0:T(8,128)S(1)}, u32[]{:S(2)}, u32[]{:S(2)}) collective-permute-start(f32[8,32,128]{2,1,0:T(8,128)S(1)} %get-tuple-element.86), channel_id=1, source_target_pairs={{0,8},{4,12},{8,0},{12,4},{1,9},{5,13},{9,1},{13,5},{2,10},{6,14},... | collective-permute-start | bytes 393224 | tf_op jit(solution)/shard_map/ppermute | solution.py:118
  33.4 1.8 %collective-permute-start.11 = (f32[16,32,128]{2,1,0:T(8,128)S(1)}, f32[16,32,128]{2,1,0:T(8,128)S(1)}, u32[]{:S(2)}, u32[]{:S(2)}) collective-permute-start(f32[16,32,128]{2,1,0:T(8,128)S(1)} %get-tuple-element.90), channel_id=1, source_target_pairs={{0,1},{1,0},{2,3},{3,2},{4,5},{5,4},{6,7},{7,6},{8,9},{9,8},{10,11... | collective-permute-start | bytes 786440 | tf_op jit(solution)/shard_map/ppermute | solution.py:531
  35.3 8.2 %collective-permute-start.13 = (f32[16,32,128]{2,1,0:T(8,128)S(1)}, f32[16,32,128]{2,1,0:T(8,128)S(1)}, u32[]{:S(2)}, u32[]{:S(2)}) collective-permute-start(f32[16,32,128]{2,1,0:T(8,128)S(1)} %add.47), channel_id=1, source_target_pairs={{0,2},{1,3},{2,0},{3,1},{4,6},{5,7},{6,4},{7,5},{8,10},{9,11},{10,... | collective-permute-start | bytes 786440 | tf_op jit(solution)/shard_map/ppermute | solution.py:479
  43.5 1.6 %collective-permute-start.14 = (f32[16,32,128]{2,1,0:T(8,128)S(1)}, f32[16,32,128]{2,1,0:T(8,128)S(1)}, u32[]{:S(2)}, u32[]{:S(2)}) collective-permute-start(f32[16,32,128]{2,1,0:T(8,128)S(1)} %add.49.refs_3_), channel_id=1, source_target_pairs={{0,1},{1,0},{2,3},{3,2},{4,5},{5,4},{6,7},{7,6},{8,9},{9,8},{10,11... | collective-permute-start | bytes 786440 | tf_op jit(solution)/shard_map/ppermute | solution.py:537
  46.5 8.3 %collective-permute-start.15 = (f32[8,32,128]{2,1,0:T(8,128)S(1)}, f32[8,32,128]{2,1,0:T(8,128)S(1)}, u32[]{:S(2)}, u32[]{:S(2)}) collective-permute-start(f32[8,32,128]{2,1,0:T(8,128)S(1)} %get-tuple-element.98), channel_id=1, source_target_pairs={{0,4},{8,12},{4,0},{12,8},{1,5},{9,13},{5,1},{13,9},{2,6},{10,14},... | collective-permute-start | bytes 393224 | tf_op jit(solution)/shard_map/ppermute | solution.py:118
  46.6 9.2 %collective-permute-start.12 = (f32[16,32,128]{2,1,0:T(8,128)S(1)}, f32[16,32,128]{2,1,0:T(8,128)S(1)}, u32[]{:S(2)}, u32[]{:S(2)}) collective-permute-start(f32[16,32,128]{2,1,0:T(8,128)S(1)} %get-tuple-element.95), channel_id=1, source_target_pairs={{0,1},{1,0},{2,3},{3,2},{4,5},{5,4},{6,7},{7,6},{8,9},{9,8},{10,11... | collective-permute-start | bytes 786440 | tf_op jit(solution)/shard_map/ppermute | solution.py:541
  46.8 12.3 %collective-permute-start.17 = (f32[8,32,128]{2,1,0:T(8,128)S(1)}, f32[8,32,128]{2,1,0:T(8,128)S(1)}, u32[]{:S(2)}, u32[]{:S(2)}) collective-permute-start(f32[8,32,128]{2,1,0:T(8,128)S(1)} %get-tuple-element.101), channel_id=1, source_target_pairs={{4,8},{0,12},{8,4},{12,0},{5,9},{1,13},{9,5},{13,1},{6,10},{2,14},... | collective-permute-start | bytes 393224 | tf_op jit(solution)/shard_map/ppermute | solution.py:118
  48.2 14.2 %collective-permute-start.19 = (f32[8,32,128]{2,1,0:T(8,128)S(1)}, f32[8,32,128]{2,1,0:T(8,128)S(1)}, u32[]{:S(2)}, u32[]{:S(2)}) collective-permute-start(f32[8,32,128]{2,1,0:T(8,128)S(1)} %get-tuple-element.105), channel_id=1, source_target_pairs={{0,8},{4,12},{8,0},{12,4},{1,9},{5,13},{9,1},{13,5},{2,10},{6,14},... | collective-permute-start | bytes 393224 | tf_op jit(solution)/shard_map/ppermute | solution.py:118
  55.8 6.4 %collective-permute-start.16 = (f32[16,32,128]{2,1,0:T(8,128)S(1)}, f32[16,32,128]{2,1,0:T(8,128)S(1)}, u32[]{:S(2)}, u32[]{:S(2)}) collective-permute-start(f32[16,32,128]{2,1,0:T(8,128)S(1)} %add.50), channel_id=1, source_target_pairs={{0,2},{1,3},{2,0},{3,1},{4,6},{5,7},{6,4},{7,5},{8,10},{9,11},{10,... | collective-permute-start | bytes 786440 | tf_op jit(solution)/shard_map/ppermute | solution.py:479
  65.5 7.9 %collective-permute-start.22 = (f32[8,32,128]{2,1,0:T(8,128)S(1)}, f32[8,32,128]{2,1,0:T(8,128)S(1)}, u32[]{:S(2)}, u32[]{:S(2)}) collective-permute-start(f32[8,32,128]{2,1,0:T(8,128)S(1)} %get-tuple-element.110), channel_id=1, source_target_pairs={{0,4},{8,12},{4,0},{12,8},{1,5},{9,13},{5,1},{13,9},{2,6},{10,14},... | collective-permute-start | bytes 393224 | tf_op jit(solution)/shard_map/ppermute | solution.py:118
  66.6 6.3 %collective-permute-start.23 = (f32[64,128]{1,0:T(8,128)S(1)}, f32[64,128]{1,0:T(8,128)S(1)}, u32[]{:S(2)}, u32[]{:S(2)}) collective-permute-start(f32[64,128]{1,0:T(8,128)S(1)} %cross.1), channel_id=1, source_target_pairs={{0,4},{4,0},{8,12},{12,8},{1,5},{5,1},{9,13},{13,9},{2,6},{6,2},{1... | collective-permute-start | bytes 98312 | tf_op jit(solution)/shard_map/ppermute | solution.py:139
  68.7 5.7 %collective-permute-start.24 = (f32[16,32,128]{2,1,0:T(8,128)S(1)}, f32[16,32,128]{2,1,0:T(8,128)S(1)}, u32[]{:S(2)}, u32[]{:S(2)}) collective-permute-start(f32[16,32,128]{2,1,0:T(8,128)S(1)} %get-tuple-element.115), channel_id=1, source_target_pairs={{0,1},{1,0},{2,3},{3,2},{4,5},{5,4},{6,7},{7,6},{8,9},{9,8},{10,11... | collective-permute-start | bytes 786440 | tf_op jit(solution)/shard_map/ppermute | solution.py:552
  68.7 16.2 %collective-permute-start.20 = (f32[8,32,128]{2,1,0:T(8,128)S(1)}, f32[8,32,128]{2,1,0:T(8,128)S(1)}, u32[]{:S(2)}, u32[]{:S(2)}) collective-permute-start(f32[8,32,128]{2,1,0:T(8,128)S(1)} %get-tuple-element.108), channel_id=1, source_target_pairs={{0,8},{4,12},{8,0},{12,4},{1,9},{5,13},{9,1},{13,5},{2,10},{6,14},... | collective-permute-start | bytes 393224 | tf_op jit(solution)/shard_map/ppermute | solution.py:118
  68.7 9.6 %collective-permute-start.21 = (f32[8,32,128]{2,1,0:T(8,128)S(1)}, f32[8,32,128]{2,1,0:T(8,128)S(1)}, u32[]{:S(2)}, u32[]{:S(2)}) collective-permute-start(f32[8,32,128]{2,1,0:T(8,128)S(1)} %get-tuple-element.109), channel_id=1, source_target_pairs={{4,8},{0,12},{8,4},{12,0},{5,9},{1,13},{9,5},{13,1},{6,10},{2,14},... | collective-permute-start | bytes 393224 | tf_op jit(solution)/shard_map/ppermute | solution.py:118
  73.0 11.9 %collective-permute-start.25 = (f32[64,128]{1,0:T(8,128)S(1)}, f32[64,128]{1,0:T(8,128)S(1)}, u32[]{:S(2)}, u32[]{:S(2)}) collective-permute-start(f32[64,128]{1,0:T(8,128)S(1)} %add.52), channel_id=1, source_target_pairs={{0,8},{4,12},{8,0},{12,4},{1,9},{5,13},{9,1},{13,5},{2,10},{6,14},... | collective-permute-start | bytes 98312 | tf_op jit(solution)/shard_map/ppermute | solution.py:148
  74.5 11.6 %collective-permute-start.28 = (f32[16,32,128]{2,1,0:T(8,128)S(1)}, f32[16,32,128]{2,1,0:T(8,128)S(1)}, u32[]{:S(2)}, u32[]{:S(2)}) collective-permute-start(f32[16,32,128]{2,1,0:T(8,128)S(1)} %add.53), channel_id=1, source_target_pairs={{0,2},{1,3},{2,0},{3,1},{4,6},{5,7},{6,4},{7,5},{8,10},{9,11},{10,... | collective-permute-start | bytes 786440 | tf_op jit(solution)/shard_map/ppermute | solution.py:479
  85.9 1.6 %collective-permute-start.26 = (f32[16,32,128]{2,1,0:T(8,128)S(1)}, f32[16,32,128]{2,1,0:T(8,128)S(1)}, u32[]{:S(2)}, u32[]{:S(2)}) collective-permute-start(f32[16,32,128]{2,1,0:T(8,128)S(1)} %get-tuple-element.121), channel_id=1, source_target_pairs={{0,1},{1,0},{2,3},{3,2},{4,5},{5,4},{6,7},{7,6},{8,9},{9,8},{10,11... | collective-permute-start | bytes 786440 | tf_op jit(solution)/shard_map/ppermute | solution.py:564
  86.1 7.0 %collective-permute-start.29 = (f32[16,32,128]{2,1,0:T(8,128)S(1)}, f32[16,32,128]{2,1,0:T(8,128)S(1)}, u32[]{:S(2)}, u32[]{:S(2)}) collective-permute-start(f32[16,32,128]{2,1,0:T(8,128)S(1)} %add.56.mine_ref), channel_id=1, source_target_pairs={{0,1},{1,0},{2,3},{3,2},{4,5},{5,4},{6,7},{7,6},{8,9},{9,8},{10,11... | collective-permute-start | bytes 786440 | tf_op jit(solution)/shard_map/ppermute | solution.py:561
  87.6 8.8 %collective-permute-start.27 = (f32[16,32,128]{2,1,0:T(8,128)S(1)}, f32[16,32,128]{2,1,0:T(8,128)S(1)}, u32[]{:S(2)}, u32[]{:S(2)}) collective-permute-start(f32[16,32,128]{2,1,0:T(8,128)S(1)} %add.55), channel_id=1, source_target_pairs={{0,2},{1,3},{2,0},{3,1},{4,6},{5,7},{6,4},{7,5},{8,10},{9,11},{10,... | collective-permute-start | bytes 786440 | tf_op jit(solution)/shard_map/ppermute | solution.py:479
  96.4 3.3 %collective-permute-start.30 = (f32[16,32,128]{2,1,0:T(8,128)S(1)}, f32[16,32,128]{2,1,0:T(8,128)S(1)}, u32[]{:S(2)}, u32[]{:S(2)}) collective-permute-start(f32[16,32,128]{2,1,0:T(8,128)S(1)} %add.57.mine_ref), channel_id=1, source_target_pairs={{0,1},{1,0},{2,3},{3,2},{4,5},{5,4},{6,7},{7,6},{8,9},{9,8},{10,11... | collective-permute-start | bytes 786440 | tf_op jit(solution)/shard_map/ppermute | solution.py:571
  102.4 4.6 %collective-permute-start.31 = (f32[64,192]{1,0:T(8,128)S(1)}, f32[64,192]{1,0:T(8,128)S(1)}, u32[]{:S(2)}, u32[]{:S(2)}) collective-permute-start(f32[64,192]{1,0:T(8,128)S(1)} %get-tuple-element.136), channel_id=1, source_target_pairs={{0,4},{4,0},{8,12},{12,8},{1,5},{5,1},{9,13},{13,9},{2,6},{6,2},{1... | collective-permute-start | bytes 147464 | tf_op jit(solution)/shard_map/ppermute | solution.py:139
  106.9 6.1 %collective-permute-start.32 = (f32[64,192]{1,0:T(8,128)S(1)}, f32[64,192]{1,0:T(8,128)S(1)}, u32[]{:S(2)}, u32[]{:S(2)}) collective-permute-start(f32[64,192]{1,0:T(8,128)S(1)} %add.58), channel_id=1, source_target_pairs={{0,8},{4,12},{8,0},{12,4},{1,9},{5,13},{9,1},{13,5},{2,10},{6,14},... | collective-permute-start | bytes 147464 | tf_op jit(solution)/shard_map/ppermute | solution.py:148
  (5 other events, 28.1 us)

commit v5 on v4

--- a/solution.py
+++ b/solution.py
@@ -44,11 +44,12 @@
     return contract(left, jnp.concatenate([m1, m1, m2], axis=axis), tb=transposed)
 
 
-def wide_product(coef, blocks):
-    c1, c2, c3 = pieces(coef, 3)
-    z1, z2, z3 = pieces(jnp.concatenate(blocks, axis=1), 3)
-    left = jnp.concatenate([c1, c1, c1, c2, c2, c3], axis=1)
-    out = contract(left, jnp.concatenate([z1, z2, z3, z1, z2, z1], axis=0))
+def wide_product(coef, blocks, terms=6):
+    pairs = [(0, 0), (0, 1), (1, 0), (1, 1)] if terms == 4 else [(0, 0), (0, 1), (0, 2), (1, 0), (1, 1), (2, 0)]
+    c = pieces(coef, terms // 2)
+    z = pieces(jnp.concatenate(blocks, axis=1), terms // 2)
+    left = jnp.concatenate([c[m] for m, _ in pairs], axis=1)
+    out = contract(left, jnp.concatenate([z[m] for _, m in pairs], axis=0))
     width = blocks[0].shape[1]
     return [out[:, n * width : (n + 1) * width] for n in range(len(blocks))]
 
@@ -111,7 +112,7 @@
                     break
             else:
                 rounds.append({"used": used, "pairs": pairs, "kinds": [(hop, parity)]})
-    return rounds
+    return rounds[::-1]
 
 
 def exchange(block, axis, pairs):
@@ -234,18 +235,16 @@
                 acc_ref[i] += direct[n * part : (n + 1) * part]
                 acc_ref[j] += mirror[n * part : (n + 1) * part]
 
-    def prepare_body(rows_hbm, cols_hbm, x_hbm, diag_hbm, tiles_hbm, *refs):
-        x_ref, split_ref, a_ref, b_ref, rows_ref, cols_ref, diag_ref, raw_ref, sem = refs
+    def prepare_body(x_hbm, diag_hbm, tiles_hbm, *refs):
+        x_ref, split_ref, a_ref, b_ref, diag_ref, raw_ref, sem = refs
         size = slots // 4
         copies = [
             pltpu.make_async_copy(src, dst, sem.at[n])
-            for n, (src, dst) in enumerate(
-                [(x_hbm, x_ref), (diag_hbm, diag_ref), (rows_hbm, rows_ref), (cols_hbm, cols_ref)]
-            )
+            for n, (src, dst) in enumerate([(x_hbm, x_ref), (diag_hbm, diag_ref)])
         ]
         tile_copies = [
             pltpu.make_async_copy(
-                tiles_hbm.at[0, 0, pl.ds(n * size, size)], raw_ref.at[pl.ds(n * size, size)], sem.at[4 + n]
+                tiles_hbm.at[0, 0, pl.ds(n * size, size)], raw_ref.at[pl.ds(n * size, size)], sem.at[2 + n]
             )
             for n in range(4)
         ]
@@ -261,10 +260,9 @@
         d = ((diag_ref[...] - SHIFT) * first)[:, None, :]
         a_ref[...] = x_ref[:, :part] * d
         b_ref[...] = x_ref[:, part:] * d
-        own_sum([a_ref, b_ref], x_ref, split_ref, rows_ref, cols_ref)
-
-    def own_body(rows_ref, cols_ref, x_ref, split_ref, prior_ref, acc_ref):
-        own_sum([acc_ref], x_ref, split_ref, rows_ref, cols_ref)
+
+    def own_body(rows_ref, cols_ref, x_ref, split_ref, *refs):
+        own_sum(refs[len(refs) // 2 :], x_ref, split_ref, rows_ref, cols_ref)
 
     def pack(place_ref, rows_ref, counts_ref, asked_refs, x_ref, split_ref, outs):
         for p in range(count):
@@ -383,6 +381,9 @@
     def identity():
         eye = lax.broadcasted_iota(jnp.int32, square, 0) == lax.broadcasted_iota(jnp.int32, square, 1)
         return eye.astype(F32)
+
+    def lower_part():
+        return lax.broadcasted_iota(jnp.int32, square, 0) >= lax.broadcasted_iota(jnp.int32, square, 1)
 
     def second_body(gram_ref, inverse_ref, cross_ref, lower_ref, coef_ref, gain_ref):
         start_inv = inverse_ref[...]
@@ -440,15 +441,24 @@
                 w_ref[n + k] = w
                 ws.append(w)
             total += gram_step(ws, [[q_refs[side][m], q_refs[side][m + 1]], ws])
-        out_ref[:, : 2 * width] = total
-        out_ref[:, 2 * width :] = norm_refs[0][...] + norm_refs[1][...]
+        norm = norm_refs[0][...] + norm_refs[1][...]
+        out_ref[:width, :width] = total[:, :width]
+        out_ref[:width, width:] = jnp.where(lower_part(), total[:, width:], norm)
+        out_ref[width:, :] = jnp.zeros((8, 2 * width), F32)
+        out_ref[width:, :width] = jnp.broadcast_to(
+            jnp.sum(norm * identity(), axis=0, keepdims=True), (8, width)
+        )
 
     def fourth_body(gram_ref, cross_ref, lower_ref, coef_ref):
-        cross = gram_ref[:, :width]
-        norm = gram_ref[:, 2 * width :]
+        cross = gram_ref[:width, :width]
+        packed = gram_ref[:width, width:]
+        flipped = packed.T
+        squares = jnp.where(lower_part(), packed, flipped)
+        norm = jnp.where(lower_part(), flipped, packed)
+        norm = jnp.where(identity() > 0, gram_ref[width : width + 1, :width], norm)
         taken = cross + SHIFT * (norm - identity())
         mixed = dot(taken, cross, tb=True)
-        squared = gram_ref[:, width : 2 * width] - mixed - mixed.T + dot(dot(taken, norm), taken, tb=True)
+        squared = squares - mixed - mixed.T + dot(dot(taken, norm), taken, tb=True)
         upper, inverse = factor(squared)
         cross_ref[...] = taken + SHIFT * identity()
         lower_ref[...] = upper.T
@@ -463,7 +473,7 @@
             side, at = divmod(n, half)
             q_ref = (low_ref, high_ref)[side]
             stacks = [jnp.concatenate([w_ref[n + k], q_ref[at + k]], axis=0) for k in range(2)]
-            for m, out in zip((n, n + 1), wide_product(coef_ref[...], stacks)):
+            for m, out in zip((n, n + 1), wide_product(coef_ref[...], stacks, 4)):
                 out_ref[m] = out
 
     swap = [(i, i ^ 1) for i in range(lanes)]
@@ -490,30 +500,33 @@
         )(place, tile_rows, slot_counts, *asked, mine, other, diagonal, split)
         return y, acc, spread(sent)
 
-    def own(acc, y):
-        return call(own_body, [chunk], [SMEM] * 2 + [VMEM] * 3, name="own", aliases={4: 0})(
-            tile_rows, tile_cols, y, split, acc
-        )[0]
+    def own(y, *accs):
+        return call(
+            own_body,
+            [chunk] * len(accs),
+            [SMEM] * 2 + [VMEM] * (2 + len(accs)),
+            name="own",
+            aliases={4 + n: n for n in range(len(accs))},
+        )(tile_rows, tile_cols, y, split, *accs)
 
     asked = [exchange(tile_cols, "res", entry["pairs"]) for entry in rounds]
     x, split, acc_a, acc_b = call(
         prepare_body,
         [full, split_shape, chunk, chunk],
-        [HBM] * 5,
+        [HBM] * 3,
         [
-            pltpu.SMEM(tile_rows.shape, jnp.int32),
-            pltpu.SMEM(tile_cols.shape, jnp.int32),
             pltpu.VMEM(diagonal.shape, F32),
             pltpu.VMEM((slots, length, length), F32),
-            pltpu.SemaphoreType.DMA((8,)),
+            pltpu.SemaphoreType.DMA((6,)),
         ],
         name="prepare",
-    )(*[pinned(v) for v in (tile_rows, tile_cols, start_block, diagonal, hess_tiles)])
+    )(*[pinned(v) for v in (start_block, diagonal, hess_tiles)])
     sent = call(
         send_body, [packet] * (2 * count), [SMEM] * (3 + count) + [VMEM] * 2, name="send"
     )(place, tile_rows, slot_counts, *asked, x, split)
     got_a = spread(sent[:count])
     sent_b = list(sent[count:])
+    acc_a, acc_b = own(x, after(acc_a, sent[0]), acc_b)
     for n in range(2):
         acc_a = join(acc_a, got_a, groups[n])
         acc_a, x, *gated = lax.optimization_barrier((acc_a, x, *[sent_b[p] for p in groups[n]]))
@@ -541,7 +554,7 @@
     core = lax.ppermute(give_b, "vec", swap)
     acc_a = join(acc_a, got_a, groups[0])
     mine_b = keep_b + after(core, acc_a)
-    acc_a = own(after(acc_a, mine_b), y_a)
+    (acc_a,) = own(y_a, after(acc_a, mine_b))
     acc_a = join(acc_a, got_a, groups[1])
     mine_b = across(mine_b, acc_a)
     other_b = lax.ppermute(mine_b, "vec", swap)
@@ -550,7 +563,7 @@
 
     (gram,) = call(cross_body, [(width, 2 * width)], [VMEM] * 3, name="cross")(x, y_a, y_b)
     core = lax.ppermute(give_a, "vec", swap)
-    acc_b = own(after(acc_b, gram), y_b)
+    (acc_b,) = own(y_b, after(acc_b, gram))
     acc_b = join(acc_b, got_b, groups[0])
     mine_a = keep_a + after(core, acc_b)
     cross_gram = start_sum(gram, "res")
@@ -572,7 +585,7 @@
     w_high, q_high, norm_high = blend(1, mine_a, other_a, after(coef, mine_b))
     w, gram = call(
         third_body,
-        [full, (width, 3 * width)],
+        [full, (width + 8, 2 * width)],
         [SMEM] + [VMEM] * 9,
         [pltpu.VMEM(chunk, F32)],
         name="third",

time: 119 us -> 120 us (level)
    ppermute x3, waiting for transfers between devices: 13.9 us -> 4.38 us  [end_sum(): got = lax.ppermute(block, axis, [(i, i ^ step) for i in range(size)])]
    ppermute x15, waiting for transfers between devices: 13.4 us -> 21.8 us  [exchange(): lax.ppermute(block, axis, [(a, b) for a, b in pairs] + [(b, a) for a, b i...]
    ppermute x4, waiting for transfers between devices: 2.47 us -> 6.02 us  [across(): got = lax.ppermute(mine, 'vec', [(i, i ^ step) for i in range(lanes)])]
    ppermute x15, starting transfers between devices: 23 us -> 20.3 us  [exchange(): lax.ppermute(block, axis, [(a, b) for a, b in pairs] + [(b, a) for a, b i...]
    ppermute x3, starting transfers between devices: 0.88 us -> 3.53 us  [end_sum(): got = lax.ppermute(block, axis, [(i, i ^ step) for i in range(size)])]
    pallas_call x4 -> x5, Pallas kernels: 9.82 us -> 10.5 us  [the longest x3 5.46 us: own(): call(own_body, [chunk] * len(accs), [SMEM] * 2 + [VMEM] * (2 + len(accs))...]
  transfers between devices with their start and end apart: 33 -> 33, of which waited for: 15 -> 14; matrix products, arithmetic and copies ran while one was open for 1% -> 1% of each run, Pallas kernels for 28% -> 29%
where the time goes in v5:
time: 120 us
  Pallas kernels  47.3 us (39%)
  waiting for transfers between devices  36.3 us (30%)
  starting transfers between devices  34 us (28%)
    ppermute x15, waiting for transfers between devices, exchange(): lax.ppermute(block, axis, [(a, b) for a, b in pairs] + [(b, a) for a, b i...  21.8 us
    ppermute x15, starting transfers between devices, exchange(): lax.ppermute(block, axis, [(a, b) for a, b in pairs] + [(b, a) for a, b i...  20.3 us
    pallas_call x12, Pallas kernels, join(): call(body, [halfchunk] * 2 if last else [chunk], [SMEM] * (3 + size) + [V...  11.7 us
    pallas_call x2, Pallas kernels, blend(): call(body, [halffull, halffull, square], [SMEM] + [VMEM] * 6, [pltpu.VMEM...  6.51 us
    ppermute x4, starting transfers between devices, across(): got = lax.ppermute(mine, 'vec', [(i, i ^ step) for i in range(lanes)])  6.23 us
    ppermute x4, waiting for transfers between devices, across(): got = lax.ppermute(mine, 'vec', [(i, i ^ step) for i in range(lanes)])  6.02 us
    pallas_call x3, Pallas kernels, own(): call(own_body, [chunk] * len(accs), [SMEM] * 2 + [VMEM] * (2 + len(accs))...  5.46 us
    ppermute x3, waiting for transfers between devices, end_sum(): got = lax.ppermute(block, axis, [(i, i ^ step) for i in range(size)])  4.38 us
  transfers between devices with their start and end apart: 33, of which 14 were waited for; matrix products, arithmetic and copies ran while one was open for 1% of the time, Pallas kernels for 29%

profile of v5, /device:TPU:0, one launch (start us, length us, event | category | flops | bytes accessed | tf_op | source)
XLA Modules:
  0.0 119.8 jit_solution(9218900219388715471)
XLA Ops:
  0.6 3.1 %collective-permute-start = (s32[1,1,44]{2,1,0:T(1,128)}, s32[1,1,44]{2,1,0:T(1,128)S(1)}, u32[]{:S(2)}, u32[]{:S(2)}) collective-permute-start(s32[1,1,44]{2,1,0:T(1,128)} %cols_ref.5), channel_id=1, source_target_pairs={{0,4},{8,12},{4,0},{12,8},{1,5},{9,13},{5,1},{13,9},{2,6},{10,14},... | collective-permute-start | bytes 536 | tf_op jit(solution)/shard_map/ppermute | solution.py:119
  3.7 2.6 %collective-permute-start.1 = (s32[1,1,44]{2,1,0:T(1,128)}, s32[1,1,44]{2,1,0:T(1,128)S(1)}, u32[]{:S(2)}, u32[]{:S(2)}) collective-permute-start(s32[1,1,44]{2,1,0:T(1,128)} %cols_ref.5), channel_id=1, source_target_pairs={{0,8},{4,12},{8,0},{12,4},{1,9},{5,13},{9,1},{13,5},{2,10},{6,14},... | collective-permute-start | bytes 536 | tf_op jit(solution)/shard_map/ppermute | solution.py:119
  7.1 2.3 %prepare.1 = (f32[32,64,128]{2,1,0:T(8,128)S(1)}, bf16[44,2,128,128]{3,2,1,0:T(8,128)(2,1)S(1)}, f32[32,32,128]{2,1,0:T(8,128)S(1)}, f32[32,32,128]{2,1,0:T(8,128)S(1)}) custom-call(f32[32,64,128]{2,1,0:T(8,128)} %x_hbm.1, f32[32,128]{1,0:T(8,128)} %refs_5_.3, f32[1,1,44,128,128]{4,3,2,1,0:T(8,128)} %tiles_hbm.1), custom_call_target="tpu_custom_call" | custom-call | tf_op jit(solution)/shard_map/prepare/pallas_call | solution.py:513
  9.4 2.4 %collective-permute-done.2.refs_1_.refs_0_ = s32[1,1,44]{2,1,0:T(1,128)S(1)} collective-permute-done((s32[1,1,44]{2,1,0:T(1,128)}, s32[1,1,44]{2,1,0:T(1,128)S(1)}, u32[]{:S(2)}, u32[]{:S(2)}) %collective-permute-start.2) | collective-permute-done | bytes 208 | tf_op jit(solution)/shard_map/ppermute | solution.py:119
  14.6 3.1 %collective-permute-start.4 = (f32[8,32,128]{2,1,0:T(8,128)S(1)}, f32[8,32,128]{2,1,0:T(8,128)S(1)}, u32[]{:S(2)}, u32[]{:S(2)}) collective-permute-start(f32[8,32,128]{2,1,0:T(8,128)S(1)} %get-tuple-element.79), channel_id=1, source_target_pairs={{4,8},{0,12},{8,4},{12,0},{5,9},{1,13},{9,5},{13,1},{6,10},{2,14},... | collective-permute-start | bytes 393224 | tf_op jit(solution)/shard_map/ppermute | solution.py:119
  17.7 2.0 %own.3 = (f32[32,32,128]{2,1,0:T(8,128)S(1)}, f32[32,32,128]{2,1,0:T(8,128)S(1)}) custom-call(s32[1,1,44]{2,1,0:T(1,128)S(1)} %copy-done.1, s32[1,1,44]{2,1,0:T(1,128)S(1)} %copy-done.2, f32[32,64,128]{2,1,0:T(8,128)S(1)} %get-tuple-element.119.refs_3_.x_ref, ...), custom_call_target="tpu_custom_call", output_to_operand_aliasing={{0}: (4, {}), {1}: (5, {})} | custom-call | tf_op jit(solution)/shard_map/own/pallas_call | solution.py:504
  19.7 3.8 %collective-permute-done.5.refs_1_ = f32[8,32,128]{2,1,0:T(8,128)S(1)} collective-permute-done((f32[8,32,128]{2,1,0:T(8,128)S(1)}, f32[8,32,128]{2,1,0:T(8,128)S(1)}, u32[]{:S(2)}, u32[]{:S(2)}) %collective-permute-start.5) | collective-permute-done | bytes 131104 | tf_op jit(solution)/shard_map/ppermute | solution.py:119
  27.5 2.1 %collective-permute-start.9 = (f32[8,32,128]{2,1,0:T(8,128)S(1)}, f32[8,32,128]{2,1,0:T(8,128)S(1)}, u32[]{:S(2)}, u32[]{:S(2)}) collective-permute-start(f32[8,32,128]{2,1,0:T(8,128)S(1)} %get-tuple-element.94), channel_id=1, source_target_pairs={{0,8},{4,12},{8,0},{12,4},{1,9},{5,13},{9,1},{13,5},{2,10},{6,14},... | collective-permute-start | bytes 393224 | tf_op jit(solution)/shard_map/ppermute | solution.py:119
  32.4 6.1 %collective-permute-done.9.refs_1_ = f32[8,32,128]{2,1,0:T(8,128)S(1)} collective-permute-done((f32[8,32,128]{2,1,0:T(8,128)S(1)}, f32[8,32,128]{2,1,0:T(8,128)S(1)}, u32[]{:S(2)}, u32[]{:S(2)}) %collective-permute-start.9) | collective-permute-done | bytes 131104 | tf_op jit(solution)/shard_map/ppermute | solution.py:119
  39.5 1.6 %collective-permute-start.13 = (f32[16,32,128]{2,1,0:T(8,128)S(1)}, f32[16,32,128]{2,1,0:T(8,128)S(1)}, u32[]{:S(2)}, u32[]{:S(2)}) collective-permute-start(f32[16,32,128]{2,1,0:T(8,128)S(1)} %add.47), channel_id=1, source_target_pairs={{0,2},{1,3},{2,0},{3,1},{4,6},{5,7},{6,4},{7,5},{8,10},{9,11},{10,... | collective-permute-start | bytes 786440 | tf_op jit(solution)/shard_map/ppermute | solution.py:489
  41.1 3.0 %first.1.inverse_ref = f32[64,64]{1,0:T(8,128)S(1)} custom-call(f32[64,64]{1,0:T(8,128)S(1)} %add.48.gram_ref), custom_call_target="tpu_custom_call" | custom-call | tf_op jit(solution)/shard_map/first/pallas_call | solution.py:547
  50.6 2.0 %collective-permute-start.19 = (f32[8,32,128]{2,1,0:T(8,128)S(1)}, f32[8,32,128]{2,1,0:T(8,128)S(1)}, u32[]{:S(2)}, u32[]{:S(2)}) collective-permute-start(f32[8,32,128]{2,1,0:T(8,128)S(1)} %get-tuple-element.111), channel_id=1, source_target_pairs={{0,4},{8,12},{4,0},{12,8},{1,5},{9,13},{5,1},{13,9},{2,6},{10,14},... | collective-permute-start | bytes 393224 | tf_op jit(solution)/shard_map/ppermute | solution.py:119
  52.6 7.3 %collective-permute-done.15.refs_1_ = f32[8,32,128]{2,1,0:T(8,128)S(1)} collective-permute-done((f32[8,32,128]{2,1,0:T(8,128)S(1)}, f32[8,32,128]{2,1,0:T(8,128)S(1)}, u32[]{:S(2)}, u32[]{:S(2)}) %collective-permute-start.15) | collective-permute-done | bytes 131104 | tf_op jit(solution)/shard_map/ppermute | solution.py:119
  60.9 1.6 %collective-permute-start.16 = (f32[16,32,128]{2,1,0:T(8,128)S(1)}, f32[16,32,128]{2,1,0:T(8,128)S(1)}, u32[]{:S(2)}, u32[]{:S(2)}) collective-permute-start(f32[16,32,128]{2,1,0:T(8,128)S(1)} %add.50), channel_id=1, source_target_pairs={{0,2},{1,3},{2,0},{3,1},{4,6},{5,7},{6,4},{7,5},{8,10},{9,11},{10,... | collective-permute-start | bytes 786440 | tf_op jit(solution)/shard_map/ppermute | solution.py:489
  62.5 1.7 %own.4.refs_3_ = f32[32,32,128]{2,1,0:T(8,128)S(1)} custom-call(s32[1,1,44]{2,1,0:T(1,128)S(1)} %copy-done.1, s32[1,1,44]{2,1,0:T(1,128)S(1)} %copy-done.2, f32[32,32,128]{2,1,0:T(8,128)S(1)} %get-tuple-element.108.x_ref.a_ref, bf16[44,2,128,128]{3,2,1,0:T(8,128)(2,1)S(1)} %get-tuple-element.76.refs_4_.split_ref.refs_2_.refs_6_, ...), custom_call_target="tpu_custom_call", output_to_operand_aliasing={{}: (4, {})} | custom-call | tf_op jit(solution)/shard_map/own/pallas_call | solution.py:504
  65.2 4.0 %collective-permute-done.16 = f32[16,32,128]{2,1,0:T(8,128)S(1)} collective-permute-done((f32[16,32,128]{2,1,0:T(8,128)S(1)}, f32[16,32,128]{2,1,0:T(8,128)S(1)}, u32[]{:S(2)}, u32[]{:S(2)}) %collective-permute-start.16) | collective-permute-done | bytes 262176 | tf_op jit(solution)/shard_map/ppermute | solution.py:489
  70.8 1.6 %resend.3 = (f32[32,32,128]{2,1,0:T(8,128)S(1)}, f32[32,32,128]{2,1,0:T(8,128)S(1)}, f32[8,32,128]{2,1,0:T(8,128)S(1)}, f32[8,32,128]{2,1,0:T(8,128)S(1)}, f32[8,32,128]{2,1,0:T(8,128)S(1)}) custom-call(s32[4]{0:T(128)S(1)} %pad_add_fusion.place_ref, s32[1,1,44]{2,1,0:T(1,128)S(1)} %copy-done.1, s32[1,1,3]{2,1,0:T(1,128)S(1)} %copy-done.3, ...), custom_call_target="tpu_custom_call" | custom-call | tf_op jit(solution)/shard_map/resend/pallas_call | solution.py:495
  73.5 2.2 %collective-permute-start.23 = (f32[64,128]{1,0:T(8,128)S(1)}, f32[64,128]{1,0:T(8,128)S(1)}, u32[]{:S(2)}, u32[]{:S(2)}) collective-permute-start(f32[64,128]{1,0:T(8,128)S(1)} %cross.1), channel_id=1, source_target_pairs={{0,4},{4,0},{8,12},{12,8},{1,5},{5,1},{9,13},{13,9},{2,6},{6,2},{1... | collective-permute-start | bytes 98312 | tf_op jit(solution)/shard_map/ppermute | solution.py:140
  75.8 2.3 %collective-permute-start.21 = (f32[8,32,128]{2,1,0:T(8,128)S(1)}, f32[8,32,128]{2,1,0:T(8,128)S(1)}, u32[]{:S(2)}, u32[]{:S(2)}) collective-permute-start(f32[8,32,128]{2,1,0:T(8,128)S(1)} %get-tuple-element.115), channel_id=1, source_target_pairs={{4,8},{0,12},{8,4},{12,0},{5,9},{1,13},{9,5},{13,1},{6,10},{2,14},... | collective-permute-start | bytes 393224 | tf_op jit(solution)/shard_map/ppermute | solution.py:119
  78.1 1.7 %own.5.refs_3_ = f32[32,32,128]{2,1,0:T(8,128)S(1)} custom-call(s32[1,1,44]{2,1,0:T(1,128)S(1)} %copy-done.1, s32[1,1,44]{2,1,0:T(1,128)S(1)} %copy-done.2, f32[32,32,128]{2,1,0:T(8,128)S(1)} %get-tuple-element.117.b_ref.x_ref, bf16[44,2,128,128]{3,2,1,0:T(8,128)(2,1)S(1)} %get-tuple-element.76.refs_4_.split_ref.refs_2_.refs_6_, ...), custom_call_target="tpu_custom_call", output_to_operand_aliasing={{}: (4, {})} | custom-call | tf_op jit(solution)/shard_map/own/pallas_call | solution.py:504
  82.0 1.6 %collective-permute-start.28 = (f32[16,32,128]{2,1,0:T(8,128)S(1)}, f32[16,32,128]{2,1,0:T(8,128)S(1)}, u32[]{:S(2)}, u32[]{:S(2)}) collective-permute-start(f32[16,32,128]{2,1,0:T(8,128)S(1)} %add.53), channel_id=1, source_target_pairs={{0,2},{1,3},{2,0},{3,1},{4,6},{5,7},{6,4},{7,5},{8,10},{9,11},{10,... | collective-permute-start | bytes 786440 | tf_op jit(solution)/shard_map/ppermute | solution.py:489
  83.5 2.2 %collective-permute-done.21.refs_1_ = f32[8,32,128]{2,1,0:T(8,128)S(1)} collective-permute-done((f32[8,32,128]{2,1,0:T(8,128)S(1)}, f32[8,32,128]{2,1,0:T(8,128)S(1)}, u32[]{:S(2)}, u32[]{:S(2)}) %collective-permute-start.21) | collective-permute-done | bytes 131104 | tf_op jit(solution)/shard_map/ppermute | solution.py:119
  90.4 1.6 %collective-permute-start.27 = (f32[16,32,128]{2,1,0:T(8,128)S(1)}, f32[16,32,128]{2,1,0:T(8,128)S(1)}, u32[]{:S(2)}, u32[]{:S(2)}) collective-permute-start(f32[16,32,128]{2,1,0:T(8,128)S(1)} %add.55), channel_id=1, source_target_pairs={{0,2},{1,3},{2,0},{3,1},{4,6},{5,7},{6,4},{7,5},{8,10},{9,11},{10,... | collective-permute-start | bytes 786440 | tf_op jit(solution)/shard_map/ppermute | solution.py:489
  92.0 3.9 %second.1 = (f32[64,64]{1,0:T(8,128)S(1)}, f32[64,64]{1,0:T(8,128)S(1)}, f32[128,192]{1,0:T(8,128)S(1)}, f32[64,64]{1,0:T(8,128)S(1)}) custom-call(f32[64,128]{1,0:T(8,128)S(1)} %add.54.gram_ref, f32[64,64]{1,0:T(8,128)S(1)} %first.1.inverse_ref), custom_call_target="tpu_custom_call" | custom-call | tf_op jit(solution)/shard_map/second/pallas_call | solution.py:579
  95.9 3.3 %blend.2 = (f32[16,64,128]{2,1,0:T(8,128)S(1)}, f32[16,64,128]{2,1,0:T(8,128)S(1)}, f32[64,64]{1,0:T(8,128)S(1)}) custom-call(s32[4]{0:T(128)S(1)} %pad_add_fusion.place_ref, f32[32,64,128]{2,1,0:T(8,128)S(1)} %get-tuple-element.119.refs_3_.x_ref, f32[32,32,128]{2,1,0:T(8,128)S(1)} %get-tuple-element.108.x_ref.a_ref, ...), custom_call_target="tpu_custom_call" | custom-call | tf_op jit(solution)/shard_map/blend/pallas_call | solution.py:423
  99.3 3.3 %blend.3 = (f32[16,64,128]{2,1,0:T(8,128)S(1)}, f32[16,64,128]{2,1,0:T(8,128)S(1)}, f32[64,64]{1,0:T(8,128)S(1)}) custom-call(s32[4]{0:T(128)S(1)} %pad_add_fusion.place_ref, f32[32,64,128]{2,1,0:T(8,128)S(1)} %get-tuple-element.119.refs_3_.x_ref, f32[32,32,128]{2,1,0:T(8,128)S(1)} %get-tuple-element.108.x_ref.a_ref, ...), custom_call_target="tpu_custom_call" | custom-call | tf_op jit(solution)/shard_map/blend/pallas_call | solution.py:423
  102.6 2.8 %third.1 = (f32[32,64,128]{2,1,0:T(8,128)S(1)}, f32[72,128]{1,0:T(8,128)S(1)}) custom-call(s32[4]{0:T(128)S(1)} %pad_add_fusion.place_ref, f32[16,32,128]{2,1,0:T(8,128)S(1)} %add.57.mine_ref, f32[16,32,128]{2,1,0:T(8,128)S(1)} %collective-permute-done.30.other_ref, f32[64,64]{1,0:T(8,128)S(1)} %get-tuple-element.136.gain_ref, ...), custom_call_target="tpu_custom_call" | custom-call | tf_op jit(solution)/shard_map/third/pallas_call | solution.py:586
  106.5 2.9 %collective-permute-done.31 = f32[72,128]{1,0:T(8,128)S(1)} collective-permute-done((f32[72,128]{1,0:T(8,128)S(1)}, f32[72,128]{1,0:T(8,128)S(1)}, u32[]{:S(2)}, u32[]{:S(2)}) %collective-permute-start.31) | collective-permute-done | bytes 36896 | tf_op jit(solution)/shard_map/ppermute | solution.py:140
  109.4 1.5 %collective-permute-start.32 = (f32[72,128]{1,0:T(8,128)S(1)}, f32[72,128]{1,0:T(8,128)S(1)}, u32[]{:S(2)}, u32[]{:S(2)}) collective-permute-start(f32[72,128]{1,0:T(8,128)S(1)} %add.58), channel_id=1, source_target_pairs={{0,8},{4,12},{8,0},{12,4},{1,9},{5,13},{9,1},{13,5},{2,10},{6,14},... | collective-permute-start | bytes 110600 | tf_op jit(solution)/shard_map/ppermute | solution.py:149
  110.9 3.3 %collective-permute-done.32 = f32[72,128]{1,0:T(8,128)S(1)} collective-permute-done((f32[72,128]{1,0:T(8,128)S(1)}, f32[72,128]{1,0:T(8,128)S(1)}, u32[]{:S(2)}, u32[]{:S(2)}) %collective-permute-start.32) | collective-permute-done | bytes 36896 | tf_op jit(solution)/shard_map/ppermute | solution.py:149
  114.2 3.7 %fourth.1 = (f32[64,64]{1,0:T(8,128)S(1)}, f32[64,64]{1,0:T(8,128)S(1)}, f32[64,128]{1,0:T(8,128)S(1)}) custom-call(f32[72,128]{1,0:T(8,128)S(1)} %add.59.gram_ref), custom_call_target="tpu_custom_call" | custom-call | tf_op jit(solution)/shard_map/fourth/pallas_call | solution.py:594
  117.9 1.9 %last.1 = (f32[32,64,128]{2,1,0:T(8,128)}, f32[4,64,64]{2,1,0:T(8,128)}) custom-call(f32[32,64,128]{2,1,0:T(8,128)S(1)} %get-tuple-element.141.w_ref, f32[16,64,128]{2,1,0:T(8,128)S(1)} %get-tuple-element.139.refs_2_.low_ref, f32[16,64,128]{2,1,0:T(8,128)S(1)} %get-tuple-element.140.refs_3_.high_ref, f32[64,128]{1,0:T(8,128)S(1)} %get-tuple-element.143.coef_ref, ...), custom_call_target="tpu_custom_call" | custom-call | tf_op jit(solution)/shard_map/last/pallas_call | solution.py:597
  (86 shorter events, 30.6 us)
Async XLA Ops:
  0.6 8.8 %collective-permute-start = (s32[1,1,44]{2,1,0:T(1,128)}, s32[1,1,44]{2,1,0:T(1,128)S(1)}, u32[]{:S(2)}, u32[]{:S(2)}) collective-permute-start(s32[1,1,44]{2,1,0:T(1,128)} %cols_ref.5), channel_id=1, source_target_pairs={{0,4},{8,12},{4,0},{12,8},{1,5},{9,13},{5,1},{13,9},{2,6},{10,14},... | collective-permute-start | bytes 536 | tf_op jit(solution)/shard_map/ppermute | solution.py:119
  3.7 5.7 %collective-permute-start.1 = (s32[1,1,44]{2,1,0:T(1,128)}, s32[1,1,44]{2,1,0:T(1,128)S(1)}, u32[]{:S(2)}, u32[]{:S(2)}) collective-permute-start(s32[1,1,44]{2,1,0:T(1,128)} %cols_ref.5), channel_id=1, source_target_pairs={{0,8},{4,12},{8,0},{12,4},{1,9},{5,13},{9,1},{13,5},{2,10},{6,14},... | collective-permute-start | bytes 536 | tf_op jit(solution)/shard_map/ppermute | solution.py:119
  6.3 5.5 %collective-permute-start.2 = (s32[1,1,44]{2,1,0:T(1,128)}, s32[1,1,44]{2,1,0:T(1,128)S(1)}, u32[]{:S(2)}, u32[]{:S(2)}) collective-permute-start(s32[1,1,44]{2,1,0:T(1,128)} %cols_ref.5), channel_id=1, source_target_pairs={{4,8},{0,12},{8,4},{12,0},{5,9},{1,13},{9,5},{13,1},{6,10},{2,14},... | collective-permute-start | bytes 536 | tf_op jit(solution)/shard_map/ppermute | solution.py:119
  13.3 10.3 %collective-permute-start.5 = (f32[8,32,128]{2,1,0:T(8,128)S(1)}, f32[8,32,128]{2,1,0:T(8,128)S(1)}, u32[]{:S(2)}, u32[]{:S(2)}) collective-permute-start(f32[8,32,128]{2,1,0:T(8,128)S(1)} %get-tuple-element.80), channel_id=1, source_target_pairs={{0,8},{4,12},{8,0},{12,4},{1,9},{5,13},{9,1},{13,5},{2,10},{6,14},... | collective-permute-start | bytes 393224 | tf_op jit(solution)/shard_map/ppermute | solution.py:119
  13.3 17.2 %collective-permute-start.3 = (f32[8,32,128]{2,1,0:T(8,128)S(1)}, f32[8,32,128]{2,1,0:T(8,128)S(1)}, u32[]{:S(2)}, u32[]{:S(2)}) collective-permute-start(f32[8,32,128]{2,1,0:T(8,128)S(1)} %get-tuple-element.78), channel_id=1, source_target_pairs={{0,4},{8,12},{4,0},{12,8},{1,5},{9,13},{5,1},{13,9},{2,6},{10,14},... | collective-permute-start | bytes 393224 | tf_op jit(solution)/shard_map/ppermute | solution.py:119
  14.6 10.5 %collective-permute-start.4 = (f32[8,32,128]{2,1,0:T(8,128)S(1)}, f32[8,32,128]{2,1,0:T(8,128)S(1)}, u32[]{:S(2)}, u32[]{:S(2)}) collective-permute-start(f32[8,32,128]{2,1,0:T(8,128)S(1)} %get-tuple-element.79), channel_id=1, source_target_pairs={{4,8},{0,12},{8,4},{12,0},{5,9},{1,13},{9,5},{13,1},{6,10},{2,14},... | collective-permute-start | bytes 393224 | tf_op jit(solution)/shard_map/ppermute | solution.py:119
  25.1 4.6 %collective-permute-start.6 = (f32[64,64]{1,0:T(8,128)S(1)}, f32[64,64]{1,0:T(8,128)S(1)}, u32[]{:S(2)}, u32[]{:S(2)}) collective-permute-start(f32[64,64]{1,0:T(8,128)S(1)} %gram.1), channel_id=1, source_target_pairs={{0,4},{4,0},{8,12},{12,8},{1,5},{5,1},{9,13},{13,9},{2,6},{6,2},{1... | collective-permute-start | bytes 49160 | tf_op jit(solution)/shard_map/ppermute | solution.py:140
  26.1 18.0 %collective-permute-start.8 = (f32[8,32,128]{2,1,0:T(8,128)S(1)}, f32[8,32,128]{2,1,0:T(8,128)S(1)}, u32[]{:S(2)}, u32[]{:S(2)}) collective-permute-start(f32[8,32,128]{2,1,0:T(8,128)S(1)} %get-tuple-element.93), channel_id=1, source_target_pairs={{4,8},{0,12},{8,4},{12,0},{5,9},{1,13},{9,5},{13,1},{6,10},{2,14},... | collective-permute-start | bytes 393224 | tf_op jit(solution)/shard_map/ppermute | solution.py:119
  27.5 11.0 %collective-permute-start.9 = (f32[8,32,128]{2,1,0:T(8,128)S(1)}, f32[8,32,128]{2,1,0:T(8,128)S(1)}, u32[]{:S(2)}, u32[]{:S(2)}) collective-permute-start(f32[8,32,128]{2,1,0:T(8,128)S(1)} %get-tuple-element.94), channel_id=1, source_target_pairs={{0,8},{4,12},{8,0},{12,4},{1,9},{5,13},{9,1},{13,5},{2,10},{6,14},... | collective-permute-start | bytes 393224 | tf_op jit(solution)/shard_map/ppermute | solution.py:119
  29.6 11.4 %collective-permute-start.10 = (f32[64,64]{1,0:T(8,128)S(1)}, f32[64,64]{1,0:T(8,128)S(1)}, u32[]{:S(2)}, u32[]{:S(2)}) collective-permute-start(f32[64,64]{1,0:T(8,128)S(1)} %add.46), channel_id=1, source_target_pairs={{0,8},{4,12},{8,0},{12,4},{1,9},{5,13},{9,1},{13,5},{2,10},{6,14},... | collective-permute-start | bytes 49160 | tf_op jit(solution)/shard_map/ppermute | solution.py:149
  31.6 14.5 %collective-permute-start.7 = (f32[8,32,128]{2,1,0:T(8,128)S(1)}, f32[8,32,128]{2,1,0:T(8,128)S(1)}, u32[]{:S(2)}, u32[]{:S(2)}) collective-permute-start(f32[8,32,128]{2,1,0:T(8,128)S(1)} %get-tuple-element.92), channel_id=1, source_target_pairs={{0,4},{8,12},{4,0},{12,8},{1,5},{9,13},{5,1},{13,9},{2,6},{10,14},... | collective-permute-start | bytes 393224 | tf_op jit(solution)/shard_map/ppermute | solution.py:119
  32.4 7.1 %collective-permute-start.11 = (f32[16,32,128]{2,1,0:T(8,128)S(1)}, f32[16,32,128]{2,1,0:T(8,128)S(1)}, u32[]{:S(2)}, u32[]{:S(2)}) collective-permute-start(f32[16,32,128]{2,1,0:T(8,128)S(1)} %get-tuple-element.96), channel_id=1, source_target_pairs={{0,1},{1,0},{2,3},{3,2},{4,5},{5,4},{6,7},{7,6},{8,9},{9,8},{10,11... | collective-permute-start | bytes 786440 | tf_op jit(solution)/shard_map/ppermute | solution.py:544
  39.5 6.4 %collective-permute-start.13 = (f32[16,32,128]{2,1,0:T(8,128)S(1)}, f32[16,32,128]{2,1,0:T(8,128)S(1)}, u32[]{:S(2)}, u32[]{:S(2)}) collective-permute-start(f32[16,32,128]{2,1,0:T(8,128)S(1)} %add.47), channel_id=1, source_target_pairs={{0,2},{1,3},{2,0},{3,1},{4,6},{5,7},{6,4},{7,5},{8,10},{9,11},{10,... | collective-permute-start | bytes 786440 | tf_op jit(solution)/shard_map/ppermute | solution.py:489
  46.0 1.6 %collective-permute-start.14 = (f32[16,32,128]{2,1,0:T(8,128)S(1)}, f32[16,32,128]{2,1,0:T(8,128)S(1)}, u32[]{:S(2)}, u32[]{:S(2)}) collective-permute-start(f32[16,32,128]{2,1,0:T(8,128)S(1)} %add.49.refs_3_), channel_id=1, source_target_pairs={{0,1},{1,0},{2,3},{3,2},{4,5},{5,4},{6,7},{7,6},{8,9},{9,8},{10,11... | collective-permute-start | bytes 786440 | tf_op jit(solution)/shard_map/ppermute | solution.py:550
  49.0 10.8 %collective-permute-start.15 = (f32[8,32,128]{2,1,0:T(8,128)S(1)}, f32[8,32,128]{2,1,0:T(8,128)S(1)}, u32[]{:S(2)}, u32[]{:S(2)}) collective-permute-start(f32[8,32,128]{2,1,0:T(8,128)S(1)} %get-tuple-element.104), channel_id=1, source_target_pairs={{0,8},{4,12},{8,0},{12,4},{1,9},{5,13},{9,1},{13,5},{2,10},{6,14},... | collective-permute-start | bytes 393224 | tf_op jit(solution)/shard_map/ppermute | solution.py:119
  49.1 11.7 %collective-permute-start.12 = (f32[16,32,128]{2,1,0:T(8,128)S(1)}, f32[16,32,128]{2,1,0:T(8,128)S(1)}, u32[]{:S(2)}, u32[]{:S(2)}) collective-permute-start(f32[16,32,128]{2,1,0:T(8,128)S(1)} %get-tuple-element.101), channel_id=1, source_target_pairs={{0,1},{1,0},{2,3},{3,2},{4,5},{5,4},{6,7},{7,6},{8,9},{9,8},{10,11... | collective-permute-start | bytes 786440 | tf_op jit(solution)/shard_map/ppermute | solution.py:554
  49.3 14.9 %collective-permute-start.17 = (f32[8,32,128]{2,1,0:T(8,128)S(1)}, f32[8,32,128]{2,1,0:T(8,128)S(1)}, u32[]{:S(2)}, u32[]{:S(2)}) collective-permute-start(f32[8,32,128]{2,1,0:T(8,128)S(1)} %get-tuple-element.107), channel_id=1, source_target_pairs={{4,8},{0,12},{8,4},{12,0},{5,9},{1,13},{9,5},{13,1},{6,10},{2,14},... | collective-permute-start | bytes 393224 | tf_op jit(solution)/shard_map/ppermute | solution.py:119
  50.6 18.6 %collective-permute-start.19 = (f32[8,32,128]{2,1,0:T(8,128)S(1)}, f32[8,32,128]{2,1,0:T(8,128)S(1)}, u32[]{:S(2)}, u32[]{:S(2)}) collective-permute-start(f32[8,32,128]{2,1,0:T(8,128)S(1)} %get-tuple-element.111), channel_id=1, source_target_pairs={{0,4},{8,12},{4,0},{12,8},{1,5},{9,13},{5,1},{13,9},{2,6},{10,14},... | collective-permute-start | bytes 393224 | tf_op jit(solution)/shard_map/ppermute | solution.py:119
  60.9 8.2 %collective-permute-start.16 = (f32[16,32,128]{2,1,0:T(8,128)S(1)}, f32[16,32,128]{2,1,0:T(8,128)S(1)}, u32[]{:S(2)}, u32[]{:S(2)}) collective-permute-start(f32[16,32,128]{2,1,0:T(8,128)S(1)} %add.50), channel_id=1, source_target_pairs={{0,2},{1,3},{2,0},{3,1},{4,6},{5,7},{6,4},{7,5},{8,10},{9,11},{10,... | collective-permute-start | bytes 786440 | tf_op jit(solution)/shard_map/ppermute | solution.py:489
  69.2 1.6 %collective-permute-start.18 = (f32[16,32,128]{2,1,0:T(8,128)S(1)}, f32[16,32,128]{2,1,0:T(8,128)S(1)}, u32[]{:S(2)}, u32[]{:S(2)}) collective-permute-start(f32[16,32,128]{2,1,0:T(8,128)S(1)} %add.51.refs_3_), channel_id=1, source_target_pairs={{0,1},{1,0},{2,3},{3,2},{4,5},{5,4},{6,7},{7,6},{8,9},{9,8},{10,11... | collective-permute-start | bytes 786440 | tf_op jit(solution)/shard_map/ppermute | solution.py:560
  72.4 8.6 %collective-permute-start.22 = (f32[8,32,128]{2,1,0:T(8,128)S(1)}, f32[8,32,128]{2,1,0:T(8,128)S(1)}, u32[]{:S(2)}, u32[]{:S(2)}) collective-permute-start(f32[8,32,128]{2,1,0:T(8,128)S(1)} %get-tuple-element.116), channel_id=1, source_target_pairs={{0,8},{4,12},{8,0},{12,4},{1,9},{5,13},{9,1},{13,5},{2,10},{6,14},... | collective-permute-start | bytes 393224 | tf_op jit(solution)/shard_map/ppermute | solution.py:119
  73.5 6.3 %collective-permute-start.23 = (f32[64,128]{1,0:T(8,128)S(1)}, f32[64,128]{1,0:T(8,128)S(1)}, u32[]{:S(2)}, u32[]{:S(2)}) collective-permute-start(f32[64,128]{1,0:T(8,128)S(1)} %cross.1), channel_id=1, source_target_pairs={{0,4},{4,0},{8,12},{12,8},{1,5},{5,1},{9,13},{13,9},{2,6},{6,2},{1... | collective-permute-start | bytes 98312 | tf_op jit(solution)/shard_map/ppermute | solution.py:140
  75.6 6.3 %collective-permute-start.24 = (f32[16,32,128]{2,1,0:T(8,128)S(1)}, f32[16,32,128]{2,1,0:T(8,128)S(1)}, u32[]{:S(2)}, u32[]{:S(2)}) collective-permute-start(f32[16,32,128]{2,1,0:T(8,128)S(1)} %get-tuple-element.121), channel_id=1, source_target_pairs={{0,1},{1,0},{2,3},{3,2},{4,5},{5,4},{6,7},{7,6},{8,9},{9,8},{10,11... | collective-permute-start | bytes 786440 | tf_op jit(solution)/shard_map/ppermute | solution.py:565
  75.7 12.1 %collective-permute-start.20 = (f32[8,32,128]{2,1,0:T(8,128)S(1)}, f32[8,32,128]{2,1,0:T(8,128)S(1)}, u32[]{:S(2)}, u32[]{:S(2)}) collective-permute-start(f32[8,32,128]{2,1,0:T(8,128)S(1)} %get-tuple-element.114), channel_id=1, source_target_pairs={{0,4},{8,12},{4,0},{12,8},{1,5},{9,13},{5,1},{13,9},{2,6},{10,14},... | collective-permute-start | bytes 393224 | tf_op jit(solution)/shard_map/ppermute | solution.py:119
  75.8 9.9 %collective-permute-start.21 = (f32[8,32,128]{2,1,0:T(8,128)S(1)}, f32[8,32,128]{2,1,0:T(8,128)S(1)}, u32[]{:S(2)}, u32[]{:S(2)}) collective-permute-start(f32[8,32,128]{2,1,0:T(8,128)S(1)} %get-tuple-element.115), channel_id=1, source_target_pairs={{4,8},{0,12},{8,4},{12,0},{5,9},{1,13},{9,5},{13,1},{6,10},{2,14},... | collective-permute-start | bytes 393224 | tf_op jit(solution)/shard_map/ppermute | solution.py:119
  79.8 7.9 %collective-permute-start.25 = (f32[64,128]{1,0:T(8,128)S(1)}, f32[64,128]{1,0:T(8,128)S(1)}, u32[]{:S(2)}, u32[]{:S(2)}) collective-permute-start(f32[64,128]{1,0:T(8,128)S(1)} %add.52), channel_id=1, source_target_pairs={{0,8},{4,12},{8,0},{12,4},{1,9},{5,13},{9,1},{13,5},{2,10},{6,14},... | collective-permute-start | bytes 98312 | tf_op jit(solution)/shard_map/ppermute | solution.py:149
  82.0 8.1 %collective-permute-start.28 = (f32[16,32,128]{2,1,0:T(8,128)S(1)}, f32[16,32,128]{2,1,0:T(8,128)S(1)}, u32[]{:S(2)}, u32[]{:S(2)}) collective-permute-start(f32[16,32,128]{2,1,0:T(8,128)S(1)} %add.53), channel_id=1, source_target_pairs={{0,2},{1,3},{2,0},{3,1},{4,6},{5,7},{6,4},{7,5},{8,10},{9,11},{10,... | collective-permute-start | bytes 786440 | tf_op jit(solution)/shard_map/ppermute | solution.py:489
  90.1 5.8 %collective-permute-start.29 = (f32[16,32,128]{2,1,0:T(8,128)S(1)}, f32[16,32,128]{2,1,0:T(8,128)S(1)}, u32[]{:S(2)}, u32[]{:S(2)}) collective-permute-start(f32[16,32,128]{2,1,0:T(8,128)S(1)} %add.56.mine_ref), channel_id=1, source_target_pairs={{0,1},{1,0},{2,3},{3,2},{4,5},{5,4},{6,7},{7,6},{8,9},{9,8},{10,11... | collective-permute-start | bytes 786440 | tf_op jit(solution)/shard_map/ppermute | solution.py:574
  90.4 8.8 %collective-permute-start.27 = (f32[16,32,128]{2,1,0:T(8,128)S(1)}, f32[16,32,128]{2,1,0:T(8,128)S(1)}, u32[]{:S(2)}, u32[]{:S(2)}) collective-permute-start(f32[16,32,128]{2,1,0:T(8,128)S(1)} %add.55), channel_id=1, source_target_pairs={{0,2},{1,3},{2,0},{3,1},{4,6},{5,7},{6,4},{7,5},{8,10},{9,11},{10,... | collective-permute-start | bytes 786440 | tf_op jit(solution)/shard_map/ppermute | solution.py:489
  99.3 3.3 %collective-permute-start.30 = (f32[16,32,128]{2,1,0:T(8,128)S(1)}, f32[16,32,128]{2,1,0:T(8,128)S(1)}, u32[]{:S(2)}, u32[]{:S(2)}) collective-permute-start(f32[16,32,128]{2,1,0:T(8,128)S(1)} %add.57.mine_ref), channel_id=1, source_target_pairs={{0,1},{1,0},{2,3},{3,2},{4,5},{5,4},{6,7},{7,6},{8,9},{9,8},{10,11... | collective-permute-start | bytes 786440 | tf_op jit(solution)/shard_map/ppermute | solution.py:584
  105.4 4.0 %collective-permute-start.31 = (f32[72,128]{1,0:T(8,128)S(1)}, f32[72,128]{1,0:T(8,128)S(1)}, u32[]{:S(2)}, u32[]{:S(2)}) collective-permute-start(f32[72,128]{1,0:T(8,128)S(1)} %get-tuple-element.142), channel_id=1, source_target_pairs={{0,4},{4,0},{8,12},{12,8},{1,5},{5,1},{9,13},{13,9},{2,6},{6,2},{1... | collective-permute-start | bytes 110600 | tf_op jit(solution)/shard_map/ppermute | solution.py:140
  109.4 4.9 %collective-permute-start.32 = (f32[72,128]{1,0:T(8,128)S(1)}, f32[72,128]{1,0:T(8,128)S(1)}, u32[]{:S(2)}, u32[]{:S(2)}) collective-permute-start(f32[72,128]{1,0:T(8,128)S(1)} %add.58), channel_id=1, source_target_pairs={{0,8},{4,12},{8,0},{12,4},{1,9},{5,13},{9,1},{13,5},{2,10},{6,14},... | collective-permute-start | bytes 110600 | tf_op jit(solution)/shard_map/ppermute | solution.py:149
  (5 other events, 33.9 us)

commit v6 on v5

--- a/solution.py
+++ b/solution.py
@@ -112,7 +112,7 @@
                     break
             else:
                 rounds.append({"used": used, "pairs": pairs, "kinds": [(hop, parity)]})
-    return rounds[::-1]
+    return rounds
 
 
 def exchange(block, axis, pairs):
@@ -552,30 +552,29 @@
     y_a, acc_a, got_a = resend(mine_a, after(other_a, keep_b))
 
     core = lax.ppermute(give_b, "vec", swap)
-    acc_a = join(acc_a, got_a, groups[0])
-    mine_b = keep_b + after(core, acc_a)
-    (acc_a,) = own(y_a, after(acc_a, mine_b))
+    mine_b = keep_b + after(core, y_a)
+    acc_a = join(after(acc_a, mine_b), got_a, groups[2])
+    (acc_a,) = own(y_a, acc_a)
     acc_a = join(acc_a, got_a, groups[1])
     mine_b = across(mine_b, acc_a)
     other_b = lax.ppermute(mine_b, "vec", swap)
-    keep_a, give_a = join(acc_a, got_a, groups[2], last=True)
+    keep_a, give_a = join(acc_a, got_a, groups[0], last=True)
     y_b, acc_b, got_b = resend(mine_b, after(other_b, keep_a))
 
-    (gram,) = call(cross_body, [(width, 2 * width)], [VMEM] * 3, name="cross")(x, y_a, y_b)
     core = lax.ppermute(give_a, "vec", swap)
-    (acc_b,) = own(y_b, after(acc_b, gram))
-    acc_b = join(acc_b, got_b, groups[0])
-    mine_a = keep_a + after(core, acc_b)
+    mine_a = keep_a + after(core, y_b)
+    acc_b = join(after(acc_b, mine_a), got_b, groups[2])
+    (acc_b,) = own(y_b, acc_b)
+    acc_b = join(acc_b, got_b, groups[1])
+    (gram,) = call(cross_body, [(width, 2 * width)], [VMEM] * 3, name="cross")(x, y_a, after(y_b, acc_b))
     cross_gram = start_sum(gram, "res")
-    acc_b = join(after(acc_b, cross_gram, mine_a), got_b, groups[1])
-    cross_gram = end_sum(cross_gram, "res", acc_b)
-    acc_b = after(acc_b, cross_gram)
-    mine_a = across(mine_a, acc_b)
+    mine_a = across(mine_a, gram)
     other_a = lax.ppermute(mine_a, "vec", swap)
-    keep_b, give_b = join(acc_b, got_b, groups[2], last=True)
+    keep_b, give_b = join(after(acc_b, cross_gram), got_b, groups[0], last=True)
 
     core = lax.ppermute(give_b, "vec", swap)
-    mine_b = keep_b + core
+    cross_gram = end_sum(cross_gram, "res")
+    mine_b = keep_b + after(core, cross_gram)
     cross1, lower1, coef, gain = call(
         second_body, [square, square, (2 * width, 3 * width), square], [VMEM] * 2, name="second"
     )(after(cross_gram, mine_b), start_inv)

time: 120 us -> 120 us (level)
  starting transfers between devices: 34 us -> 41.2 us
  waiting for transfers between devices: 36.3 us -> 29.3 us
    ppermute x15, waiting for transfers between devices: 21.8 us -> 15.4 us  [exchange(): lax.ppermute(block, axis, [(a, b) for a, b in pairs] + [(b, a) for a, b i...]
    ppermute x15, starting transfers between devices: 20.3 us -> 26.7 us  [exchange(): lax.ppermute(block, axis, [(a, b) for a, b in pairs] + [(b, a) for a, b i...]
    ppermute x3, waiting for transfers between devices: 4.38 us -> 9.33 us  [end_sum(): got = lax.ppermute(block, axis, [(i, i ^ step) for i in range(size)])]
    ppermute x4, waiting for transfers between devices: 6.02 us -> 1.35 us  [across(): got = lax.ppermute(mine, 'vec', [(i, i ^ step) for i in range(lanes)])]
    ppermute x3, starting transfers between devices: 3.53 us -> 2.06 us  [end_sum(): got = lax.ppermute(block, axis, [(i, i ^ step) for i in range(size)])]
    ppermute x3, starting transfers between devices: 3.32 us -> 4.67 us  [start_sum(): lax.ppermute(block, axis, [(i, i ^ step) for i in range(size)])]
  transfers between devices with their start and end apart: 33 -> 33, of which waited for: 14 -> 13; matrix products, arithmetic and copies ran while one was open for 1% -> 1% of each run, Pallas kernels for 29% -> 31%
where the time goes in v6:
time: 120 us
  Pallas kernels  47.3 us (39%)
  starting transfers between devices  41.2 us (34%)
  waiting for transfers between devices  29.3 us (24%)
    ppermute x15, starting transfers between devices, exchange(): lax.ppermute(block, axis, [(a, b) for a, b in pairs] + [(b, a) for a, b i...  26.7 us
    ppermute x15, waiting for transfers between devices, exchange(): lax.ppermute(block, axis, [(a, b) for a, b in pairs] + [(b, a) for a, b i...  15.4 us
    pallas_call x12, Pallas kernels, join(): call(body, [halfchunk] * 2 if last else [chunk], [SMEM] * (3 + size) + [V...  11.9 us
    ppermute x3, waiting for transfers between devices, end_sum(): got = lax.ppermute(block, axis, [(i, i ^ step) for i in range(size)])  9.33 us
    pallas_call x2, Pallas kernels, blend(): call(body, [halffull, halffull, square], [SMEM] + [VMEM] * 6, [pltpu.VMEM...  6.5 us
    ppermute x4, starting transfers between devices, across(): got = lax.ppermute(mine, 'vec', [(i, i ^ step) for i in range(lanes)])  6.16 us
    pallas_call x3, Pallas kernels, own(): call(own_body, [chunk] * len(accs), [SMEM] * 2 + [VMEM] * (2 + len(accs))...  5.46 us
    ppermute x3, starting transfers between devices, start_sum(): lax.ppermute(block, axis, [(i, i ^ step) for i in range(size)])  4.67 us
  transfers between devices with their start and end apart: 33, of which 13 were waited for; matrix products, arithmetic and copies ran while one was open for 1% of the time, Pallas kernels for 31%

profile of v6, /device:TPU:0, one launch (start us, length us, event | category | flops | bytes accessed | tf_op | source)
XLA Modules:
  0.0 120.0 jit_solution(6093417673121212549)
XLA Ops:
  0.6 4.1 %collective-permute-start.2 = (s32[1,1,44]{2,1,0:T(1,128)}, s32[1,1,44]{2,1,0:T(1,128)S(1)}, u32[]{:S(2)}, u32[]{:S(2)}) collective-permute-start(s32[1,1,44]{2,1,0:T(1,128)} %cols_ref.5), channel_id=1, source_target_pairs={{0,8},{4,12},{8,0},{12,4},{1,9},{5,13},{9,1},{13,5},{2,10},{6,14},... | collective-permute-start | bytes 536 | tf_op jit(solution)/shard_map/ppermute | solution.py:119
  7.1 2.3 %prepare.1 = (f32[32,64,128]{2,1,0:T(8,128)S(1)}, bf16[44,2,128,128]{3,2,1,0:T(8,128)(2,1)S(1)}, f32[32,32,128]{2,1,0:T(8,128)S(1)}, f32[32,32,128]{2,1,0:T(8,128)S(1)}) custom-call(f32[32,64,128]{2,1,0:T(8,128)} %x_hbm.1, f32[32,128]{1,0:T(8,128)} %refs_5_.3, f32[1,1,44,128,128]{4,3,2,1,0:T(8,128)} %tiles_hbm.1), custom_call_target="tpu_custom_call" | custom-call | tf_op jit(solution)/shard_map/prepare/pallas_call | solution.py:513
  10.2 1.4 %send.1 = (f32[8,32,128]{2,1,0:T(8,128)S(1)}, f32[8,32,128]{2,1,0:T(8,128)S(1)}, f32[8,32,128]{2,1,0:T(8,128)S(1)}, f32[8,32,128]{2,1,0:T(8,128)S(1)}, f32[8,32,...) custom-call(s32[4]{0:T(128)S(1)} %pad_add_fusion.place_ref, s32[1,1,44]{2,1,0:T(1,128)S(1)} %copy-done.1, ...), custom_call_target="tpu_custom_call" | custom-call | tf_op jit(solution)/shard_map/send/pallas_call | solution.py:524
  13.7 2.4 %collective-permute-start.4 = (f32[8,32,128]{2,1,0:T(8,128)S(1)}, f32[8,32,128]{2,1,0:T(8,128)S(1)}, u32[]{:S(2)}, u32[]{:S(2)}) collective-permute-start(f32[8,32,128]{2,1,0:T(8,128)S(1)} %get-tuple-element.79), channel_id=1, source_target_pairs={{4,8},{0,12},{8,4},{12,0},{5,9},{1,13},{9,5},{13,1},{6,10},{2,14},... | collective-permute-start | bytes 393224 | tf_op jit(solution)/shard_map/ppermute | solution.py:119
  16.1 2.0 %own.3 = (f32[32,32,128]{2,1,0:T(8,128)S(1)}, f32[32,32,128]{2,1,0:T(8,128)S(1)}) custom-call(s32[1,1,44]{2,1,0:T(1,128)S(1)} %copy-done.1, s32[1,1,44]{2,1,0:T(1,128)S(1)} %copy-done.2, f32[32,64,128]{2,1,0:T(8,128)S(1)} %get-tuple-element.122.refs_3_.x_ref, ...), custom_call_target="tpu_custom_call", output_to_operand_aliasing={{0}: (4, {}), {1}: (5, {})} | custom-call | tf_op jit(solution)/shard_map/own/pallas_call | solution.py:504
  20.2 2.9 %collective-permute-done.4.refs_1_ = f32[8,32,128]{2,1,0:T(8,128)S(1)} collective-permute-done((f32[8,32,128]{2,1,0:T(8,128)S(1)}, f32[8,32,128]{2,1,0:T(8,128)S(1)}, u32[]{:S(2)}, u32[]{:S(2)}) %collective-permute-start.4) | collective-permute-done | bytes 131104 | tf_op jit(solution)/shard_map/ppermute | solution.py:119
  25.4 4.5 %collective-permute-start.9 = (f32[8,32,128]{2,1,0:T(8,128)S(1)}, f32[8,32,128]{2,1,0:T(8,128)S(1)}, u32[]{:S(2)}, u32[]{:S(2)}) collective-permute-start(f32[8,32,128]{2,1,0:T(8,128)S(1)} %get-tuple-element.94), channel_id=1, source_target_pairs={{0,4},{8,12},{4,0},{12,8},{1,5},{9,13},{5,1},{13,9},{2,6},{10,14},... | collective-permute-start | bytes 393224 | tf_op jit(solution)/shard_map/ppermute | solution.py:119
  31.1 2.6 %collective-permute-start.7 = (f32[8,32,128]{2,1,0:T(8,128)S(1)}, f32[8,32,128]{2,1,0:T(8,128)S(1)}, u32[]{:S(2)}, u32[]{:S(2)}) collective-permute-start(f32[8,32,128]{2,1,0:T(8,128)S(1)} %get-tuple-element.92), channel_id=1, source_target_pairs={{0,8},{4,12},{8,0},{12,4},{1,9},{5,13},{9,1},{13,5},{2,10},{6,14},... | collective-permute-start | bytes 393224 | tf_op jit(solution)/shard_map/ppermute | solution.py:119
  35.3 1.6 %collective-permute-start.13 = (f32[16,32,128]{2,1,0:T(8,128)S(1)}, f32[16,32,128]{2,1,0:T(8,128)S(1)}, u32[]{:S(2)}, u32[]{:S(2)}) collective-permute-start(f32[16,32,128]{2,1,0:T(8,128)S(1)} %add.47), channel_id=1, source_target_pairs={{0,2},{1,3},{2,0},{3,1},{4,6},{5,7},{6,4},{7,5},{8,10},{9,11},{10,... | collective-permute-start | bytes 786440 | tf_op jit(solution)/shard_map/ppermute | solution.py:489
  36.8 1.6 %collective-permute-done.10 = f32[64,64]{1,0:T(8,128)S(1)} collective-permute-done((f32[64,64]{1,0:T(8,128)S(1)}, f32[64,64]{1,0:T(8,128)S(1)}, u32[]{:S(2)}, u32[]{:S(2)}) %collective-permute-start.10) | collective-permute-done | bytes 16416 | tf_op jit(solution)/shard_map/ppermute | solution.py:149
  38.4 3.0 %first.1.inverse_ref = f32[64,64]{1,0:T(8,128)S(1)} custom-call(f32[64,64]{1,0:T(8,128)S(1)} %add.48.gram_ref), custom_call_target="tpu_custom_call" | custom-call | tf_op jit(solution)/shard_map/first/pallas_call | solution.py:547
  45.4 1.4 %resend.2 = (f32[32,32,128]{2,1,0:T(8,128)S(1)}, f32[32,32,128]{2,1,0:T(8,128)S(1)}, f32[8,32,128]{2,1,0:T(8,128)S(1)}, f32[8,32,128]{2,1,0:T(8,128)S(1)}, f32[8,32,128]{2,1,0:T(8,128)S(1)}) custom-call(s32[4]{0:T(128)S(1)} %pad_add_fusion.place_ref, s32[1,1,44]{2,1,0:T(1,128)S(1)} %copy-done.1, s32[1,1,3]{2,1,0:T(1,128)S(1)} %copy-done.3, ...), custom_call_target="tpu_custom_call" | custom-call | tf_op jit(solution)/shard_map/resend/pallas_call | solution.py:495
  47.0 1.6 %collective-permute-start.15 = (f32[16,32,128]{2,1,0:T(8,128)S(1)}, f32[16,32,128]{2,1,0:T(8,128)S(1)}, u32[]{:S(2)}, u32[]{:S(2)}) collective-permute-start(f32[16,32,128]{2,1,0:T(8,128)S(1)} %add.50), channel_id=1, source_target_pairs={{0,2},{1,3},{2,0},{3,1},{4,6},{5,7},{6,4},{7,5},{8,10},{9,11},{10,... | collective-permute-start | bytes 786440 | tf_op jit(solution)/shard_map/ppermute | solution.py:489
  48.5 2.1 %collective-permute-start.16 = (f32[8,32,128]{2,1,0:T(8,128)S(1)}, f32[8,32,128]{2,1,0:T(8,128)S(1)}, u32[]{:S(2)}, u32[]{:S(2)}) collective-permute-start(f32[8,32,128]{2,1,0:T(8,128)S(1)} %get-tuple-element.106), channel_id=1, source_target_pairs={{4,8},{0,12},{8,4},{12,0},{5,9},{1,13},{9,5},{13,1},{6,10},{2,14},... | collective-permute-start | bytes 393224 | tf_op jit(solution)/shard_map/ppermute | solution.py:119
  52.0 6.2 %collective-permute-done.17.refs_1_ = f32[8,32,128]{2,1,0:T(8,128)S(1)} collective-permute-done((f32[8,32,128]{2,1,0:T(8,128)S(1)}, f32[8,32,128]{2,1,0:T(8,128)S(1)}, u32[]{:S(2)}, u32[]{:S(2)}) %collective-permute-start.17) | collective-permute-done | bytes 131104 | tf_op jit(solution)/shard_map/ppermute | solution.py:119
  59.2 1.7 %own.4.refs_3_ = f32[32,32,128]{2,1,0:T(8,128)S(1)} custom-call(s32[1,1,44]{2,1,0:T(1,128)S(1)} %copy-done.1, s32[1,1,44]{2,1,0:T(1,128)S(1)} %copy-done.2, f32[32,32,128]{2,1,0:T(8,128)S(1)} %get-tuple-element.104.x_ref.a_ref, bf16[44,2,128,128]{3,2,1,0:T(8,128)(2,1)S(1)} %get-tuple-element.76.refs_4_.split_ref.refs_2_.refs_6_, ...), custom_call_target="tpu_custom_call", output_to_operand_aliasing={{}: (4, {})} | custom-call | tf_op jit(solution)/shard_map/own/pallas_call | solution.py:504
  66.3 3.3 %collective-permute-start.21 = (f32[8,32,128]{2,1,0:T(8,128)S(1)}, f32[8,32,128]{2,1,0:T(8,128)S(1)}, u32[]{:S(2)}, u32[]{:S(2)}) collective-permute-start(f32[8,32,128]{2,1,0:T(8,128)S(1)} %get-tuple-element.115), channel_id=1, source_target_pairs={{4,8},{0,12},{8,4},{12,0},{5,9},{1,13},{9,5},{13,1},{6,10},{2,14},... | collective-permute-start | bytes 393224 | tf_op jit(solution)/shard_map/ppermute | solution.py:119
  69.7 5.3 %collective-permute-done.22.refs_1_ = f32[8,32,128]{2,1,0:T(8,128)S(1)} collective-permute-done((f32[8,32,128]{2,1,0:T(8,128)S(1)}, f32[8,32,128]{2,1,0:T(8,128)S(1)}, u32[]{:S(2)}, u32[]{:S(2)}) %collective-permute-start.22) | collective-permute-done | bytes 131104 | tf_op jit(solution)/shard_map/ppermute | solution.py:119
  76.1 1.7 %own.5.refs_3_ = f32[32,32,128]{2,1,0:T(8,128)S(1)} custom-call(s32[1,1,44]{2,1,0:T(1,128)S(1)} %copy-done.1, s32[1,1,44]{2,1,0:T(1,128)S(1)} %copy-done.2, f32[32,32,128]{2,1,0:T(8,128)S(1)} %get-tuple-element.123.x_ref.b_ref, bf16[44,2,128,128]{3,2,1,0:T(8,128)(2,1)S(1)} %get-tuple-element.76.refs_4_.split_ref.refs_2_.refs_6_, ...), custom_call_target="tpu_custom_call", output_to_operand_aliasing={{}: (4, {})} | custom-call | tf_op jit(solution)/shard_map/own/pallas_call | solution.py:504
  79.9 2.5 %collective-permute-start.24 = (f32[64,128]{1,0:T(8,128)S(1)}, f32[64,128]{1,0:T(8,128)S(1)}, u32[]{:S(2)}, u32[]{:S(2)}) collective-permute-start(f32[64,128]{1,0:T(8,128)S(1)} %cross.1), channel_id=1, source_target_pairs={{0,4},{4,0},{8,12},{12,8},{1,5},{5,1},{9,13},{13,9},{2,6},{6,2},{1... | collective-permute-start | bytes 98312 | tf_op jit(solution)/shard_map/ppermute | solution.py:140
  82.3 1.5 %collective-permute-start.28 = (f32[16,32,128]{2,1,0:T(8,128)S(1)}, f32[16,32,128]{2,1,0:T(8,128)S(1)}, u32[]{:S(2)}, u32[]{:S(2)}) collective-permute-start(f32[16,32,128]{2,1,0:T(8,128)S(1)} %add.52), channel_id=1, source_target_pairs={{0,2},{1,3},{2,0},{3,1},{4,6},{5,7},{6,4},{7,5},{8,10},{9,11},{10,... | collective-permute-start | bytes 786440 | tf_op jit(solution)/shard_map/ppermute | solution.py:489
  86.4 3.8 %collective-permute-done.26 = f32[64,128]{1,0:T(8,128)S(1)} collective-permute-done((f32[64,128]{1,0:T(8,128)S(1)}, f32[64,128]{1,0:T(8,128)S(1)}, u32[]{:S(2)}, u32[]{:S(2)}) %collective-permute-start.26) | collective-permute-done | bytes 32800 | tf_op jit(solution)/shard_map/ppermute | solution.py:149
  90.5 1.6 %collective-permute-start.27 = (f32[16,32,128]{2,1,0:T(8,128)S(1)}, f32[16,32,128]{2,1,0:T(8,128)S(1)}, u32[]{:S(2)}, u32[]{:S(2)}) collective-permute-start(f32[16,32,128]{2,1,0:T(8,128)S(1)} %add.55), channel_id=1, source_target_pairs={{0,2},{1,3},{2,0},{3,1},{4,6},{5,7},{6,4},{7,5},{8,10},{9,11},{10,... | collective-permute-start | bytes 786440 | tf_op jit(solution)/shard_map/ppermute | solution.py:489
  92.0 3.9 %second.1 = (f32[64,64]{1,0:T(8,128)S(1)}, f32[64,64]{1,0:T(8,128)S(1)}, f32[128,192]{1,0:T(8,128)S(1)}, f32[64,64]{1,0:T(8,128)S(1)}) custom-call(f32[64,128]{1,0:T(8,128)S(1)} %add.54.gram_ref, f32[64,64]{1,0:T(8,128)S(1)} %first.1.inverse_ref), custom_call_target="tpu_custom_call" | custom-call | tf_op jit(solution)/shard_map/second/pallas_call | solution.py:578
  96.0 3.3 %blend.2 = (f32[16,64,128]{2,1,0:T(8,128)S(1)}, f32[16,64,128]{2,1,0:T(8,128)S(1)}, f32[64,64]{1,0:T(8,128)S(1)}) custom-call(s32[4]{0:T(128)S(1)} %pad_add_fusion.place_ref, f32[32,64,128]{2,1,0:T(8,128)S(1)} %get-tuple-element.122.refs_3_.x_ref, f32[32,32,128]{2,1,0:T(8,128)S(1)} %get-tuple-element.104.x_ref.a_ref, ...), custom_call_target="tpu_custom_call" | custom-call | tf_op jit(solution)/shard_map/blend/pallas_call | solution.py:423
  99.6 3.2 %blend.3 = (f32[16,64,128]{2,1,0:T(8,128)S(1)}, f32[16,64,128]{2,1,0:T(8,128)S(1)}, f32[64,64]{1,0:T(8,128)S(1)}) custom-call(s32[4]{0:T(128)S(1)} %pad_add_fusion.place_ref, f32[32,64,128]{2,1,0:T(8,128)S(1)} %get-tuple-element.122.refs_3_.x_ref, f32[32,32,128]{2,1,0:T(8,128)S(1)} %get-tuple-element.104.x_ref.a_ref, ...), custom_call_target="tpu_custom_call" | custom-call | tf_op jit(solution)/shard_map/blend/pallas_call | solution.py:423
  102.8 2.7 %third.1 = (f32[32,64,128]{2,1,0:T(8,128)S(1)}, f32[72,128]{1,0:T(8,128)S(1)}) custom-call(s32[4]{0:T(128)S(1)} %pad_add_fusion.place_ref, f32[16,32,128]{2,1,0:T(8,128)S(1)} %add.57.mine_ref, f32[16,32,128]{2,1,0:T(8,128)S(1)} %collective-permute-done.30.other_ref, f32[64,64]{1,0:T(8,128)S(1)} %get-tuple-element.136.gain_ref, ...), custom_call_target="tpu_custom_call" | custom-call | tf_op jit(solution)/shard_map/third/pallas_call | solution.py:585
  105.6 1.7 %collective-permute-start.31 = (f32[72,128]{1,0:T(8,128)S(1)}, f32[72,128]{1,0:T(8,128)S(1)}, u32[]{:S(2)}, u32[]{:S(2)}) collective-permute-start(f32[72,128]{1,0:T(8,128)S(1)} %get-tuple-element.142), channel_id=1, source_target_pairs={{0,4},{4,0},{8,12},{12,8},{1,5},{5,1},{9,13},{13,9},{2,6},{6,2},{1... | collective-permute-start | bytes 110600 | tf_op jit(solution)/shard_map/ppermute | solution.py:140
  107.3 2.3 %collective-permute-done.31 = f32[72,128]{1,0:T(8,128)S(1)} collective-permute-done((f32[72,128]{1,0:T(8,128)S(1)}, f32[72,128]{1,0:T(8,128)S(1)}, u32[]{:S(2)}, u32[]{:S(2)}) %collective-permute-start.31) | collective-permute-done | bytes 36896 | tf_op jit(solution)/shard_map/ppermute | solution.py:140
  110.5 3.9 %collective-permute-done.32 = f32[72,128]{1,0:T(8,128)S(1)} collective-permute-done((f32[72,128]{1,0:T(8,128)S(1)}, f32[72,128]{1,0:T(8,128)S(1)}, u32[]{:S(2)}, u32[]{:S(2)}) %collective-permute-start.32) | collective-permute-done | bytes 36896 | tf_op jit(solution)/shard_map/ppermute | solution.py:149
  114.5 3.7 %fourth.1 = (f32[64,64]{1,0:T(8,128)S(1)}, f32[64,64]{1,0:T(8,128)S(1)}, f32[64,128]{1,0:T(8,128)S(1)}) custom-call(f32[72,128]{1,0:T(8,128)S(1)} %add.59.gram_ref), custom_call_target="tpu_custom_call" | custom-call | tf_op jit(solution)/shard_map/fourth/pallas_call | solution.py:593
  118.2 1.9 %last.1 = (f32[32,64,128]{2,1,0:T(8,128)}, f32[4,64,64]{2,1,0:T(8,128)}) custom-call(f32[32,64,128]{2,1,0:T(8,128)S(1)} %get-tuple-element.141.w_ref, f32[16,64,128]{2,1,0:T(8,128)S(1)} %get-tuple-element.139.refs_2_.low_ref, f32[16,64,128]{2,1,0:T(8,128)S(1)} %get-tuple-element.140.refs_3_.high_ref, f32[64,128]{1,0:T(8,128)S(1)} %get-tuple-element.143.coef_ref, ...), custom_call_target="tpu_custom_call" | custom-call | tf_op jit(solution)/shard_map/last/pallas_call | solution.py:596
  (86 shorter events, 31.0 us)
Async XLA Ops:
  0.6 8.8 %collective-permute-start.2 = (s32[1,1,44]{2,1,0:T(1,128)}, s32[1,1,44]{2,1,0:T(1,128)S(1)}, u32[]{:S(2)}, u32[]{:S(2)}) collective-permute-start(s32[1,1,44]{2,1,0:T(1,128)} %cols_ref.5), channel_id=1, source_target_pairs={{0,8},{4,12},{8,0},{12,4},{1,9},{5,13},{9,1},{13,5},{2,10},{6,14},... | collective-permute-start | bytes 536 | tf_op jit(solution)/shard_map/ppermute | solution.py:119
  4.8 5.5 %collective-permute-start.1 = (s32[1,1,44]{2,1,0:T(1,128)}, s32[1,1,44]{2,1,0:T(1,128)S(1)}, u32[]{:S(2)}, u32[]{:S(2)}) collective-permute-start(s32[1,1,44]{2,1,0:T(1,128)} %cols_ref.5), channel_id=1, source_target_pairs={{4,8},{0,12},{8,4},{12,0},{5,9},{1,13},{9,5},{13,1},{6,10},{2,14},... | collective-permute-start | bytes 536 | tf_op jit(solution)/shard_map/ppermute | solution.py:119
  6.1 4.1 %collective-permute-start = (s32[1,1,44]{2,1,0:T(1,128)}, s32[1,1,44]{2,1,0:T(1,128)S(1)}, u32[]{:S(2)}, u32[]{:S(2)}) collective-permute-start(s32[1,1,44]{2,1,0:T(1,128)} %cols_ref.5), channel_id=1, source_target_pairs={{0,4},{8,12},{4,0},{12,8},{1,5},{9,13},{5,1},{13,9},{2,6},{10,14},... | collective-permute-start | bytes 536 | tf_op jit(solution)/shard_map/ppermute | solution.py:119
  11.7 6.5 %collective-permute-start.5 = (f32[8,32,128]{2,1,0:T(8,128)S(1)}, f32[8,32,128]{2,1,0:T(8,128)S(1)}, u32[]{:S(2)}, u32[]{:S(2)}) collective-permute-start(f32[8,32,128]{2,1,0:T(8,128)S(1)} %get-tuple-element.80), channel_id=1, source_target_pairs={{0,4},{8,12},{4,0},{12,8},{1,5},{9,13},{5,1},{13,9},{2,6},{10,14},... | collective-permute-start | bytes 393224 | tf_op jit(solution)/shard_map/ppermute | solution.py:119
  12.5 17.5 %collective-permute-start.3 = (f32[8,32,128]{2,1,0:T(8,128)S(1)}, f32[8,32,128]{2,1,0:T(8,128)S(1)}, u32[]{:S(2)}, u32[]{:S(2)}) collective-permute-start(f32[8,32,128]{2,1,0:T(8,128)S(1)} %get-tuple-element.78), channel_id=1, source_target_pairs={{0,8},{4,12},{8,0},{12,4},{1,9},{5,13},{9,1},{13,5},{2,10},{6,14},... | collective-permute-start | bytes 393224 | tf_op jit(solution)/shard_map/ppermute | solution.py:119
  13.7 9.4 %collective-permute-start.4 = (f32[8,32,128]{2,1,0:T(8,128)S(1)}, f32[8,32,128]{2,1,0:T(8,128)S(1)}, u32[]{:S(2)}, u32[]{:S(2)}) collective-permute-start(f32[8,32,128]{2,1,0:T(8,128)S(1)} %get-tuple-element.79), channel_id=1, source_target_pairs={{4,8},{0,12},{8,4},{12,0},{5,9},{1,13},{9,5},{13,1},{6,10},{2,14},... | collective-permute-start | bytes 393224 | tf_op jit(solution)/shard_map/ppermute | solution.py:119
  19.7 10.3 %collective-permute-start.6 = (f32[64,64]{1,0:T(8,128)S(1)}, f32[64,64]{1,0:T(8,128)S(1)}, u32[]{:S(2)}, u32[]{:S(2)}) collective-permute-start(f32[64,64]{1,0:T(8,128)S(1)} %gram.1), channel_id=1, source_target_pairs={{0,4},{4,0},{8,12},{12,8},{1,5},{5,1},{9,13},{13,9},{2,6},{6,2},{1... | collective-permute-start | bytes 49160 | tf_op jit(solution)/shard_map/ppermute | solution.py:140
  24.1 17.4 %collective-permute-start.8 = (f32[8,32,128]{2,1,0:T(8,128)S(1)}, f32[8,32,128]{2,1,0:T(8,128)S(1)}, u32[]{:S(2)}, u32[]{:S(2)}) collective-permute-start(f32[8,32,128]{2,1,0:T(8,128)S(1)} %get-tuple-element.93), channel_id=1, source_target_pairs={{4,8},{0,12},{8,4},{12,0},{5,9},{1,13},{9,5},{13,1},{6,10},{2,14},... | collective-permute-start | bytes 393224 | tf_op jit(solution)/shard_map/ppermute | solution.py:119
  25.4 8.4 %collective-permute-start.9 = (f32[8,32,128]{2,1,0:T(8,128)S(1)}, f32[8,32,128]{2,1,0:T(8,128)S(1)}, u32[]{:S(2)}, u32[]{:S(2)}) collective-permute-start(f32[8,32,128]{2,1,0:T(8,128)S(1)} %get-tuple-element.94), channel_id=1, source_target_pairs={{0,4},{8,12},{4,0},{12,8},{1,5},{9,13},{5,1},{13,9},{2,6},{10,14},... | collective-permute-start | bytes 393224 | tf_op jit(solution)/shard_map/ppermute | solution.py:119
  29.9 8.5 %collective-permute-start.10 = (f32[64,64]{1,0:T(8,128)S(1)}, f32[64,64]{1,0:T(8,128)S(1)}, u32[]{:S(2)}, u32[]{:S(2)}) collective-permute-start(f32[64,64]{1,0:T(8,128)S(1)} %add.46), channel_id=1, source_target_pairs={{0,8},{4,12},{8,0},{12,4},{1,9},{5,13},{9,1},{13,5},{2,10},{6,14},... | collective-permute-start | bytes 49160 | tf_op jit(solution)/shard_map/ppermute | solution.py:149
  31.1 12.7 %collective-permute-start.7 = (f32[8,32,128]{2,1,0:T(8,128)S(1)}, f32[8,32,128]{2,1,0:T(8,128)S(1)}, u32[]{:S(2)}, u32[]{:S(2)}) collective-permute-start(f32[8,32,128]{2,1,0:T(8,128)S(1)} %get-tuple-element.92), channel_id=1, source_target_pairs={{0,8},{4,12},{8,0},{12,4},{1,9},{5,13},{9,1},{13,5},{2,10},{6,14},... | collective-permute-start | bytes 393224 | tf_op jit(solution)/shard_map/ppermute | solution.py:119
  35.3 8.4 %collective-permute-start.13 = (f32[16,32,128]{2,1,0:T(8,128)S(1)}, f32[16,32,128]{2,1,0:T(8,128)S(1)}, u32[]{:S(2)}, u32[]{:S(2)}) collective-permute-start(f32[16,32,128]{2,1,0:T(8,128)S(1)} %add.47), channel_id=1, source_target_pairs={{0,2},{1,3},{2,0},{3,1},{4,6},{5,7},{6,4},{7,5},{8,10},{9,11},{10,... | collective-permute-start | bytes 786440 | tf_op jit(solution)/shard_map/ppermute | solution.py:489
  43.7 1.7 %collective-permute-start.14 = (f32[16,32,128]{2,1,0:T(8,128)S(1)}, f32[16,32,128]{2,1,0:T(8,128)S(1)}, u32[]{:S(2)}, u32[]{:S(2)}) collective-permute-start(f32[16,32,128]{2,1,0:T(8,128)S(1)} %add.49.refs_3_), channel_id=1, source_target_pairs={{0,1},{1,0},{2,3},{3,2},{4,5},{5,4},{6,7},{7,6},{8,9},{9,8},{10,11... | collective-permute-start | bytes 786440 | tf_op jit(solution)/shard_map/ppermute | solution.py:550
  44.9 2.1 %collective-permute-start.12 = (f32[16,32,128]{2,1,0:T(8,128)S(1)}, f32[16,32,128]{2,1,0:T(8,128)S(1)}, u32[]{:S(2)}, u32[]{:S(2)}) collective-permute-start(f32[16,32,128]{2,1,0:T(8,128)S(1)} %get-tuple-element.101), channel_id=1, source_target_pairs={{0,1},{1,0},{2,3},{3,2},{4,5},{5,4},{6,7},{7,6},{8,9},{9,8},{10,11... | collective-permute-start | bytes 786440 | tf_op jit(solution)/shard_map/ppermute | solution.py:554
  46.9 11.4 %collective-permute-start.17 = (f32[8,32,128]{2,1,0:T(8,128)S(1)}, f32[8,32,128]{2,1,0:T(8,128)S(1)}, u32[]{:S(2)}, u32[]{:S(2)}) collective-permute-start(f32[8,32,128]{2,1,0:T(8,128)S(1)} %get-tuple-element.107), channel_id=1, source_target_pairs={{0,8},{4,12},{8,0},{12,4},{1,9},{5,13},{9,1},{13,5},{2,10},{6,14},... | collective-permute-start | bytes 393224 | tf_op jit(solution)/shard_map/ppermute | solution.py:119
  47.0 14.9 %collective-permute-start.15 = (f32[16,32,128]{2,1,0:T(8,128)S(1)}, f32[16,32,128]{2,1,0:T(8,128)S(1)}, u32[]{:S(2)}, u32[]{:S(2)}) collective-permute-start(f32[16,32,128]{2,1,0:T(8,128)S(1)} %add.50), channel_id=1, source_target_pairs={{0,2},{1,3},{2,0},{3,1},{4,6},{5,7},{6,4},{7,5},{8,10},{9,11},{10,... | collective-permute-start | bytes 786440 | tf_op jit(solution)/shard_map/ppermute | solution.py:489
  48.5 12.4 %collective-permute-start.16 = (f32[8,32,128]{2,1,0:T(8,128)S(1)}, f32[8,32,128]{2,1,0:T(8,128)S(1)}, u32[]{:S(2)}, u32[]{:S(2)}) collective-permute-start(f32[8,32,128]{2,1,0:T(8,128)S(1)} %get-tuple-element.106), channel_id=1, source_target_pairs={{4,8},{0,12},{8,4},{12,0},{5,9},{1,13},{9,5},{13,1},{6,10},{2,14},... | collective-permute-start | bytes 393224 | tf_op jit(solution)/shard_map/ppermute | solution.py:119
  50.7 11.4 %collective-permute-start.19 = (f32[8,32,128]{2,1,0:T(8,128)S(1)}, f32[8,32,128]{2,1,0:T(8,128)S(1)}, u32[]{:S(2)}, u32[]{:S(2)}) collective-permute-start(f32[8,32,128]{2,1,0:T(8,128)S(1)} %get-tuple-element.111), channel_id=1, source_target_pairs={{0,4},{8,12},{4,0},{12,8},{1,5},{9,13},{5,1},{13,9},{2,6},{10,14},... | collective-permute-start | bytes 393224 | tf_op jit(solution)/shard_map/ppermute | solution.py:119
  62.0 1.7 %collective-permute-start.18 = (f32[16,32,128]{2,1,0:T(8,128)S(1)}, f32[16,32,128]{2,1,0:T(8,128)S(1)}, u32[]{:S(2)}, u32[]{:S(2)}) collective-permute-start(f32[16,32,128]{2,1,0:T(8,128)S(1)} %add.51.refs_3_), channel_id=1, source_target_pairs={{0,1},{1,0},{2,3},{3,2},{4,5},{5,4},{6,7},{7,6},{8,9},{9,8},{10,11... | collective-permute-start | bytes 786440 | tf_op jit(solution)/shard_map/ppermute | solution.py:560
  63.1 2.1 %collective-permute-start.23 = (f32[16,32,128]{2,1,0:T(8,128)S(1)}, f32[16,32,128]{2,1,0:T(8,128)S(1)}, u32[]{:S(2)}, u32[]{:S(2)}) collective-permute-start(f32[16,32,128]{2,1,0:T(8,128)S(1)} %get-tuple-element.119), channel_id=1, source_target_pairs={{0,1},{1,0},{2,3},{3,2},{4,5},{5,4},{6,7},{7,6},{8,9},{9,8},{10,11... | collective-permute-start | bytes 786440 | tf_op jit(solution)/shard_map/ppermute | solution.py:564
  65.1 9.9 %collective-permute-start.22 = (f32[8,32,128]{2,1,0:T(8,128)S(1)}, f32[8,32,128]{2,1,0:T(8,128)S(1)}, u32[]{:S(2)}, u32[]{:S(2)}) collective-permute-start(f32[8,32,128]{2,1,0:T(8,128)S(1)} %get-tuple-element.117), channel_id=1, source_target_pairs={{0,8},{4,12},{8,0},{12,4},{1,9},{5,13},{9,1},{13,5},{2,10},{6,14},... | collective-permute-start | bytes 393224 | tf_op jit(solution)/shard_map/ppermute | solution.py:119
  65.2 19.0 %collective-permute-start.20 = (f32[8,32,128]{2,1,0:T(8,128)S(1)}, f32[8,32,128]{2,1,0:T(8,128)S(1)}, u32[]{:S(2)}, u32[]{:S(2)}) collective-permute-start(f32[8,32,128]{2,1,0:T(8,128)S(1)} %get-tuple-element.114), channel_id=1, source_target_pairs={{0,4},{8,12},{4,0},{12,8},{1,5},{9,13},{5,1},{13,9},{2,6},{10,14},... | collective-permute-start | bytes 393224 | tf_op jit(solution)/shard_map/ppermute | solution.py:119
  66.3 11.6 %collective-permute-start.21 = (f32[8,32,128]{2,1,0:T(8,128)S(1)}, f32[8,32,128]{2,1,0:T(8,128)S(1)}, u32[]{:S(2)}, u32[]{:S(2)}) collective-permute-start(f32[8,32,128]{2,1,0:T(8,128)S(1)} %get-tuple-element.115), channel_id=1, source_target_pairs={{4,8},{0,12},{8,4},{12,0},{5,9},{1,13},{9,5},{13,1},{6,10},{2,14},... | collective-permute-start | bytes 393224 | tf_op jit(solution)/shard_map/ppermute | solution.py:119
  79.9 4.4 %collective-permute-start.24 = (f32[64,128]{1,0:T(8,128)S(1)}, f32[64,128]{1,0:T(8,128)S(1)}, u32[]{:S(2)}, u32[]{:S(2)}) collective-permute-start(f32[64,128]{1,0:T(8,128)S(1)} %cross.1), channel_id=1, source_target_pairs={{0,4},{4,0},{8,12},{12,8},{1,5},{5,1},{9,13},{13,9},{2,6},{6,2},{1... | collective-permute-start | bytes 98312 | tf_op jit(solution)/shard_map/ppermute | solution.py:140
  82.3 8.0 %collective-permute-start.28 = (f32[16,32,128]{2,1,0:T(8,128)S(1)}, f32[16,32,128]{2,1,0:T(8,128)S(1)}, u32[]{:S(2)}, u32[]{:S(2)}) collective-permute-start(f32[16,32,128]{2,1,0:T(8,128)S(1)} %add.52), channel_id=1, source_target_pairs={{0,2},{1,3},{2,0},{3,1},{4,6},{5,7},{6,4},{7,5},{8,10},{9,11},{10,... | collective-permute-start | bytes 786440 | tf_op jit(solution)/shard_map/ppermute | solution.py:489
  85.3 5.1 %collective-permute-start.25 = (f32[16,32,128]{2,1,0:T(8,128)S(1)}, f32[16,32,128]{2,1,0:T(8,128)S(1)}, u32[]{:S(2)}, u32[]{:S(2)}) collective-permute-start(f32[16,32,128]{2,1,0:T(8,128)S(1)} %get-tuple-element.126), channel_id=1, source_target_pairs={{0,1},{1,0},{2,3},{3,2},{4,5},{5,4},{6,7},{7,6},{8,9},{9,8},{10,11... | collective-permute-start | bytes 786440 | tf_op jit(solution)/shard_map/ppermute | solution.py:575
  85.4 4.9 %collective-permute-start.26 = (f32[64,128]{1,0:T(8,128)S(1)}, f32[64,128]{1,0:T(8,128)S(1)}, u32[]{:S(2)}, u32[]{:S(2)}) collective-permute-start(f32[64,128]{1,0:T(8,128)S(1)} %add.53), channel_id=1, source_target_pairs={{0,8},{4,12},{8,0},{12,4},{1,9},{5,13},{9,1},{13,5},{2,10},{6,14},... | collective-permute-start | bytes 98312 | tf_op jit(solution)/shard_map/ppermute | solution.py:149
  90.3 5.6 %collective-permute-start.29 = (f32[16,32,128]{2,1,0:T(8,128)S(1)}, f32[16,32,128]{2,1,0:T(8,128)S(1)}, u32[]{:S(2)}, u32[]{:S(2)}) collective-permute-start(f32[16,32,128]{2,1,0:T(8,128)S(1)} %add.56.mine_ref), channel_id=1, source_target_pairs={{0,1},{1,0},{2,3},{3,2},{4,5},{5,4},{6,7},{7,6},{8,9},{9,8},{10,11... | collective-permute-start | bytes 786440 | tf_op jit(solution)/shard_map/ppermute | solution.py:572
  90.5 8.8 %collective-permute-start.27 = (f32[16,32,128]{2,1,0:T(8,128)S(1)}, f32[16,32,128]{2,1,0:T(8,128)S(1)}, u32[]{:S(2)}, u32[]{:S(2)}) collective-permute-start(f32[16,32,128]{2,1,0:T(8,128)S(1)} %add.55), channel_id=1, source_target_pairs={{0,2},{1,3},{2,0},{3,1},{4,6},{5,7},{6,4},{7,5},{8,10},{9,11},{10,... | collective-permute-start | bytes 786440 | tf_op jit(solution)/shard_map/ppermute | solution.py:489
  99.3 3.5 %collective-permute-start.30 = (f32[16,32,128]{2,1,0:T(8,128)S(1)}, f32[16,32,128]{2,1,0:T(8,128)S(1)}, u32[]{:S(2)}, u32[]{:S(2)}) collective-permute-start(f32[16,32,128]{2,1,0:T(8,128)S(1)} %add.57.mine_ref), channel_id=1, source_target_pairs={{0,1},{1,0},{2,3},{3,2},{4,5},{5,4},{6,7},{7,6},{8,9},{9,8},{10,11... | collective-permute-start | bytes 786440 | tf_op jit(solution)/shard_map/ppermute | solution.py:583
  105.6 4.0 %collective-permute-start.31 = (f32[72,128]{1,0:T(8,128)S(1)}, f32[72,128]{1,0:T(8,128)S(1)}, u32[]{:S(2)}, u32[]{:S(2)}) collective-permute-start(f32[72,128]{1,0:T(8,128)S(1)} %get-tuple-element.142), channel_id=1, source_target_pairs={{0,4},{4,0},{8,12},{12,8},{1,5},{5,1},{9,13},{13,9},{2,6},{6,2},{1... | collective-permute-start | bytes 110600 | tf_op jit(solution)/shard_map/ppermute | solution.py:140
  109.6 4.9 %collective-permute-start.32 = (f32[72,128]{1,0:T(8,128)S(1)}, f32[72,128]{1,0:T(8,128)S(1)}, u32[]{:S(2)}, u32[]{:S(2)}) collective-permute-start(f32[72,128]{1,0:T(8,128)S(1)} %add.58), channel_id=1, source_target_pairs={{0,8},{4,12},{8,0},{12,4},{1,9},{5,13},{9,1},{13,5},{2,10},{6,14},... | collective-permute-start | bytes 110600 | tf_op jit(solution)/shard_map/ppermute | solution.py:149
  (5 other events, 29.2 us)

commit v7 on v5

--- a/solution.py
+++ b/solution.py
@@ -112,7 +112,7 @@
                     break
             else:
                 rounds.append({"used": used, "pairs": pairs, "kinds": [(hop, parity)]})
-    return rounds[::-1]
+    return rounds
 
 
 def exchange(block, axis, pairs):
@@ -406,9 +406,7 @@
     def blend(side, mine, other, coef):
         def body(place_ref, x_ref, a_ref, b_ref, mine_ref, other_ref, coef_ref, w_ref, q_ref, out_ref, z_ref):
             settle(place_ref, mine_ref, other_ref, z_ref)
-            total = jnp.zeros(square, F32)
             for n in range(0, half, 2):
-                qs = []
                 stacks = [
                     jnp.concatenate([ref[side * half + m] for ref in (x_ref, a_ref, b_ref, z_ref)], axis=0)
                     for m in (n, n + 1)
@@ -416,7 +414,9 @@
                 for m, both in zip((n, n + 1), wide_product(coef_ref[:, : 2 * width + part], stacks)):
                     w_ref[m] = both[:width]
                     q_ref[m] = both[width:]
-                    qs.append(both[width:])
+            total = jnp.zeros(square, F32)
+            for n in range(0, half, 2):
+                qs = [q_ref[n], q_ref[n + 1]]
                 total += gram_step(qs, [qs])
             out_ref[...] = total
 
@@ -432,14 +432,14 @@
         prior_refs, q_refs, norm_refs = refs[0:2], refs[2:4], refs[4:6]
         w_ref, out_ref, z_ref = refs[6:]
         settle(place_ref, mine_ref, other_ref, z_ref)
+        for n in range(0, rows, 2):
+            side, m = divmod(n, half)
+            for k, w in enumerate(wide_product(gain_ref[:, part:], [z_ref[n], z_ref[n + 1]])):
+                w_ref[n + k] = w + prior_refs[side][m + k]
         total = jnp.zeros((width, 2 * width), F32)
         for n in range(0, rows, 2):
             side, m = divmod(n, half)
-            ws = []
-            for k, w in enumerate(wide_product(gain_ref[:, part:], [z_ref[n], z_ref[n + 1]])):
-                w = w + prior_refs[side][m + k]
-                w_ref[n + k] = w
-                ws.append(w)
+            ws = [w_ref[n], w_ref[n + 1]]
             total += gram_step(ws, [[q_refs[side][m], q_refs[side][m + 1]], ws])
         norm = norm_refs[0][...] + norm_refs[1][...]
         out_ref[:width, :width] = total[:, :width]
@@ -552,13 +552,13 @@
     y_a, acc_a, got_a = resend(mine_a, after(other_a, keep_b))
 
     core = lax.ppermute(give_b, "vec", swap)
-    acc_a = join(acc_a, got_a, groups[0])
-    mine_b = keep_b + after(core, acc_a)
-    (acc_a,) = own(y_a, after(acc_a, mine_b))
+    mine_b = keep_b + after(core, y_a)
+    acc_a = join(after(acc_a, mine_b), got_a, groups[2])
+    (acc_a,) = own(y_a, acc_a)
     acc_a = join(acc_a, got_a, groups[1])
     mine_b = across(mine_b, acc_a)
     other_b = lax.ppermute(mine_b, "vec", swap)
-    keep_a, give_a = join(acc_a, got_a, groups[2], last=True)
+    keep_a, give_a = join(acc_a, got_a, groups[0], last=True)
     y_b, acc_b, got_b = resend(mine_b, after(other_b, keep_a))
 
     (gram,) = call(cross_body, [(width, 2 * width)], [VMEM] * 3, name="cross")(x, y_a, y_b)
@@ -580,16 +580,16 @@
         second_body, [square, square, (2 * width, 3 * width), square], [VMEM] * 2, name="second"
     )(after(cross_gram, mine_b), start_inv)
     w_low, q_low, norm_low = blend(0, mine_a, other_a, coef)
-    mine_b = across(mine_b, norm_low)
+    w_high, q_high, norm_high = blend(1, mine_a, other_a, coef)
+    mine_b = across(mine_b, norm_low, norm_high)
     other_b = lax.ppermute(mine_b, "vec", swap)
-    w_high, q_high, norm_high = blend(1, mine_a, other_a, after(coef, mine_b))
     w, gram = call(
         third_body,
         [full, (width + 8, 2 * width)],
         [SMEM] + [VMEM] * 9,
         [pltpu.VMEM(chunk, F32)],
         name="third",
-    )(place, mine_b, after(other_b, norm_high), gain, w_low, w_high, q_low, q_high, norm_low, norm_high)
+    )(place, mine_b, other_b, gain, w_low, w_high, q_low, q_high, norm_low, norm_high)
     gram = all_sum(gram, "res")
     cross2, lower2, coef = call(
         fourth_body, [square, square, (width, 2 * width)], [VMEM], name="fourth"

time: 120 us -> 115 us (0.958)
  Pallas kernels: 47.3 us -> 43.5 us
  waiting for transfers between devices: 36.3 us -> 33.4 us
  starting transfers between devices: 34 us -> 35.9 us
    ppermute x15, waiting for transfers between devices: 21.8 us -> 13.5 us  [exchange(): lax.ppermute(block, axis, [(a, b) for a, b in pairs] + [(b, a) for a, b i...]
    ppermute x3, waiting for transfers between devices: 4.38 us -> 11.1 us  [end_sum(): got = lax.ppermute(block, axis, [(i, i ^ step) for i in range(size)])]
    ppermute x4, waiting for transfers between devices: 6.02 us -> 2.25 us  [across(): got = lax.ppermute(mine, 'vec', [(i, i ^ step) for i in range(lanes)])]
    ppermute x15, starting transfers between devices: 20.3 us -> 24 us  [exchange(): lax.ppermute(block, axis, [(a, b) for a, b in pairs] + [(b, a) for a, b i...]
    pallas_call x2, Pallas kernels: 6.51 us -> 3.43 us  [blend(): call(body, [halffull, halffull, square], [SMEM] + [VMEM] * 6, [pltpu.VMEM...]
    ppermute x3, starting transfers between devices: 3.53 us -> 1.48 us  [end_sum(): got = lax.ppermute(block, axis, [(i, i ^ step) for i in range(size)])]
    ppermute x2, waiting for transfers between devices: 0.48 us -> 2 us  [local(): other_b = lax.ppermute(mine_b, 'vec', swap)]
where the time goes in v7:
time: 115 us
  Pallas kernels  43.5 us (38%)
  starting transfers between devices  35.9 us (31%)
  waiting for transfers between devices  33.4 us (29%)
    ppermute x15, starting transfers between devices, exchange(): lax.ppermute(block, axis, [(a, b) for a, b in pairs] + [(b, a) for a, b i...  24 us
    ppermute x15, waiting for transfers between devices, exchange(): lax.ppermute(block, axis, [(a, b) for a, b in pairs] + [(b, a) for a, b i...  13.5 us
    pallas_call x12, Pallas kernels, join(): call(body, [halfchunk] * 2 if last else [chunk], [SMEM] * (3 + size) + [V...  11.7 us
    ppermute x3, waiting for transfers between devices, end_sum(): got = lax.ppermute(block, axis, [(i, i ^ step) for i in range(size)])  11.1 us
    ppermute x4, starting transfers between devices, across(): got = lax.ppermute(mine, 'vec', [(i, i ^ step) for i in range(lanes)])  6.23 us
    pallas_call x3, Pallas kernels, own(): call(own_body, [chunk] * len(accs), [SMEM] * 2 + [VMEM] * (2 + len(accs))...  5.47 us
    pallas_call x1, Pallas kernels, local(): call(second_body, [square, square, (2 * width, 3 * width), square], [VMEM...  3.94 us
    pallas_call x1, Pallas kernels, local(): call(fourth_body, [square, square, (width, 2 * width)], [VMEM], name='fou...  3.7 us
  transfers between devices with their start and end apart: 33, of which 14 were waited for; matrix products, arithmetic and copies ran while one was open for 1% of the time, Pallas kernels for 29%

profile of v7, /device:TPU:0, one launch (start us, length us, event | category | flops | bytes accessed | tf_op | source)
XLA Modules:
  0.0 114.9 jit_solution(13638207567163801864)
XLA Ops:
  0.6 4.1 %collective-permute-start = (s32[1,1,44]{2,1,0:T(1,128)}, s32[1,1,44]{2,1,0:T(1,128)S(1)}, u32[]{:S(2)}, u32[]{:S(2)}) collective-permute-start(s32[1,1,44]{2,1,0:T(1,128)} %cols_ref.5), channel_id=1, source_target_pairs={{0,8},{4,12},{8,0},{12,4},{1,9},{5,13},{9,1},{13,5},{2,10},{6,14},... | collective-permute-start | bytes 536 | tf_op jit(solution)/shard_map/ppermute | solution.py:119
  4.8 1.6 %collective-permute-start.1 = (s32[1,1,44]{2,1,0:T(1,128)}, s32[1,1,44]{2,1,0:T(1,128)S(1)}, u32[]{:S(2)}, u32[]{:S(2)}) collective-permute-start(s32[1,1,44]{2,1,0:T(1,128)} %cols_ref.5), channel_id=1, source_target_pairs={{0,4},{8,12},{4,0},{12,8},{1,5},{9,13},{5,1},{13,9},{2,6},{10,14},... | collective-permute-start | bytes 536 | tf_op jit(solution)/shard_map/ppermute | solution.py:119
  7.1 2.3 %prepare.1 = (f32[32,64,128]{2,1,0:T(8,128)S(1)}, bf16[44,2,128,128]{3,2,1,0:T(8,128)(2,1)S(1)}, f32[32,32,128]{2,1,0:T(8,128)S(1)}, f32[32,32,128]{2,1,0:T(8,128)S(1)}) custom-call(f32[32,64,128]{2,1,0:T(8,128)} %x_hbm.1, f32[32,128]{1,0:T(8,128)} %refs_5_.3, f32[1,1,44,128,128]{4,3,2,1,0:T(8,128)} %tiles_hbm.1), custom_call_target="tpu_custom_call" | custom-call | tf_op jit(solution)/shard_map/prepare/pallas_call | solution.py:513
  9.4 2.4 %collective-permute-done.2.refs_1_.refs_0_ = s32[1,1,44]{2,1,0:T(1,128)S(1)} collective-permute-done((s32[1,1,44]{2,1,0:T(1,128)}, s32[1,1,44]{2,1,0:T(1,128)S(1)}, u32[]{:S(2)}, u32[]{:S(2)}) %collective-permute-start.2) | collective-permute-done | bytes 208 | tf_op jit(solution)/shard_map/ppermute | solution.py:119
  14.6 3.1 %collective-permute-start.4 = (f32[8,32,128]{2,1,0:T(8,128)S(1)}, f32[8,32,128]{2,1,0:T(8,128)S(1)}, u32[]{:S(2)}, u32[]{:S(2)}) collective-permute-start(f32[8,32,128]{2,1,0:T(8,128)S(1)} %get-tuple-element.77), channel_id=1, source_target_pairs={{4,8},{0,12},{8,4},{12,0},{5,9},{1,13},{9,5},{13,1},{6,10},{2,14},... | collective-permute-start | bytes 393224 | tf_op jit(solution)/shard_map/ppermute | solution.py:119
  17.7 2.0 %own.3 = (f32[32,32,128]{2,1,0:T(8,128)S(1)}, f32[32,32,128]{2,1,0:T(8,128)S(1)}) custom-call(s32[1,1,44]{2,1,0:T(1,128)S(1)} %copy-done.1, s32[1,1,44]{2,1,0:T(1,128)S(1)} %copy-done.2, f32[32,64,128]{2,1,0:T(8,128)S(1)} %get-tuple-element.117.refs_3_.x_ref, ...), custom_call_target="tpu_custom_call", output_to_operand_aliasing={{0}: (4, {}), {1}: (5, {})} | custom-call | tf_op jit(solution)/shard_map/own/pallas_call | solution.py:504
  21.3 1.7 %collective-permute-done.4.refs_1_ = f32[8,32,128]{2,1,0:T(8,128)S(1)} collective-permute-done((f32[8,32,128]{2,1,0:T(8,128)S(1)}, f32[8,32,128]{2,1,0:T(8,128)S(1)}, u32[]{:S(2)}, u32[]{:S(2)}) %collective-permute-start.4) | collective-permute-done | bytes 131104 | tf_op jit(solution)/shard_map/ppermute | solution.py:119
  23.9 1.9 %collective-permute-start.8 = (f32[8,32,128]{2,1,0:T(8,128)S(1)}, f32[8,32,128]{2,1,0:T(8,128)S(1)}, u32[]{:S(2)}, u32[]{:S(2)}) collective-permute-start(f32[8,32,128]{2,1,0:T(8,128)S(1)} %get-tuple-element.91), channel_id=1, source_target_pairs={{4,8},{0,12},{8,4},{12,0},{5,9},{1,13},{9,5},{13,1},{6,10},{2,14},... | collective-permute-start | bytes 393224 | tf_op jit(solution)/shard_map/ppermute | solution.py:119
  25.8 3.8 %collective-permute-start.9 = (f32[8,32,128]{2,1,0:T(8,128)S(1)}, f32[8,32,128]{2,1,0:T(8,128)S(1)}, u32[]{:S(2)}, u32[]{:S(2)}) collective-permute-start(f32[8,32,128]{2,1,0:T(8,128)S(1)} %get-tuple-element.92), channel_id=1, source_target_pairs={{0,4},{8,12},{4,0},{12,8},{1,5},{9,13},{5,1},{13,9},{2,6},{10,14},... | collective-permute-start | bytes 393224 | tf_op jit(solution)/shard_map/ppermute | solution.py:119
  35.0 1.6 %collective-permute-start.13 = (f32[16,32,128]{2,1,0:T(8,128)S(1)}, f32[16,32,128]{2,1,0:T(8,128)S(1)}, u32[]{:S(2)}, u32[]{:S(2)}) collective-permute-start(f32[16,32,128]{2,1,0:T(8,128)S(1)} %add.47), channel_id=1, source_target_pairs={{0,2},{1,3},{2,0},{3,1},{4,6},{5,7},{6,4},{7,5},{8,10},{9,11},{10,... | collective-permute-start | bytes 786440 | tf_op jit(solution)/shard_map/ppermute | solution.py:489
  37.2 3.0 %first.1.inverse_ref = f32[64,64]{1,0:T(8,128)S(1)} custom-call(f32[64,64]{1,0:T(8,128)S(1)} %add.48.gram_ref), custom_call_target="tpu_custom_call" | custom-call | tf_op jit(solution)/shard_map/first/pallas_call | solution.py:547
  41.1 2.2 %collective-permute-done.13 = f32[16,32,128]{2,1,0:T(8,128)S(1)} collective-permute-done((f32[16,32,128]{2,1,0:T(8,128)S(1)}, f32[16,32,128]{2,1,0:T(8,128)S(1)}, u32[]{:S(2)}, u32[]{:S(2)}) %collective-permute-start.13) | collective-permute-done | bytes 262176 | tf_op jit(solution)/shard_map/ppermute | solution.py:489
  47.6 1.6 %collective-permute-start.15 = (f32[16,32,128]{2,1,0:T(8,128)S(1)}, f32[16,32,128]{2,1,0:T(8,128)S(1)}, u32[]{:S(2)}, u32[]{:S(2)}) collective-permute-start(f32[16,32,128]{2,1,0:T(8,128)S(1)} %add.50), channel_id=1, source_target_pairs={{0,2},{1,3},{2,0},{3,1},{4,6},{5,7},{6,4},{7,5},{8,10},{9,11},{10,... | collective-permute-start | bytes 786440 | tf_op jit(solution)/shard_map/ppermute | solution.py:489
  49.1 1.9 %collective-permute-start.16 = (f32[8,32,128]{2,1,0:T(8,128)S(1)}, f32[8,32,128]{2,1,0:T(8,128)S(1)}, u32[]{:S(2)}, u32[]{:S(2)}) collective-permute-start(f32[8,32,128]{2,1,0:T(8,128)S(1)} %get-tuple-element.104), channel_id=1, source_target_pairs={{4,8},{0,12},{8,4},{12,0},{5,9},{1,13},{9,5},{13,1},{6,10},{2,14},... | collective-permute-start | bytes 393224 | tf_op jit(solution)/shard_map/ppermute | solution.py:119
  51.7 6.9 %collective-permute-done.17.refs_1_ = f32[8,32,128]{2,1,0:T(8,128)S(1)} collective-permute-done((f32[8,32,128]{2,1,0:T(8,128)S(1)}, f32[8,32,128]{2,1,0:T(8,128)S(1)}, u32[]{:S(2)}, u32[]{:S(2)}) %collective-permute-start.17) | collective-permute-done | bytes 131104 | tf_op jit(solution)/shard_map/ppermute | solution.py:119
  59.5 1.7 %own.4.refs_3_ = f32[32,32,128]{2,1,0:T(8,128)S(1)} custom-call(s32[1,1,44]{2,1,0:T(1,128)S(1)} %copy-done.1, s32[1,1,44]{2,1,0:T(1,128)S(1)} %copy-done.2, f32[32,32,128]{2,1,0:T(8,128)S(1)} %get-tuple-element.102.x_ref.a_ref, bf16[44,2,128,128]{3,2,1,0:T(8,128)(2,1)S(1)} %get-tuple-element.74.refs_4_.split_ref.refs_2_.refs_6_, ...), custom_call_target="tpu_custom_call", output_to_operand_aliasing={{}: (4, {})} | custom-call | tf_op jit(solution)/shard_map/own/pallas_call | solution.py:504
  63.9 1.6 %resend.3 = (f32[32,32,128]{2,1,0:T(8,128)S(1)}, f32[32,32,128]{2,1,0:T(8,128)S(1)}, f32[8,32,128]{2,1,0:T(8,128)S(1)}, f32[8,32,128]{2,1,0:T(8,128)S(1)}, f32[8,32,128]{2,1,0:T(8,128)S(1)}) custom-call(s32[4]{0:T(128)S(1)} %pad_add_fusion.place_ref, s32[1,1,44]{2,1,0:T(1,128)S(1)} %copy-done.1, s32[1,1,3]{2,1,0:T(1,128)S(1)} %copy-done.3, ...), custom_call_target="tpu_custom_call" | custom-call | tf_op jit(solution)/shard_map/resend/pallas_call | solution.py:495
  67.0 1.7 %collective-permute-start.23 = (f32[64,128]{1,0:T(8,128)S(1)}, f32[64,128]{1,0:T(8,128)S(1)}, u32[]{:S(2)}, u32[]{:S(2)}) collective-permute-start(f32[64,128]{1,0:T(8,128)S(1)} %cross.1), channel_id=1, source_target_pairs={{0,4},{4,0},{8,12},{12,8},{1,5},{5,1},{9,13},{13,9},{2,6},{6,2},{1... | collective-permute-start | bytes 98312 | tf_op jit(solution)/shard_map/ppermute | solution.py:140
  69.0 2.4 %collective-permute-start.21 = (f32[8,32,128]{2,1,0:T(8,128)S(1)}, f32[8,32,128]{2,1,0:T(8,128)S(1)}, u32[]{:S(2)}, u32[]{:S(2)}) collective-permute-start(f32[8,32,128]{2,1,0:T(8,128)S(1)} %get-tuple-element.113), channel_id=1, source_target_pairs={{4,8},{0,12},{8,4},{12,0},{5,9},{1,13},{9,5},{13,1},{6,10},{2,14},... | collective-permute-start | bytes 393224 | tf_op jit(solution)/shard_map/ppermute | solution.py:119
  71.4 1.7 %own.5.refs_3_ = f32[32,32,128]{2,1,0:T(8,128)S(1)} custom-call(s32[1,1,44]{2,1,0:T(1,128)S(1)} %copy-done.1, s32[1,1,44]{2,1,0:T(1,128)S(1)} %copy-done.2, f32[32,32,128]{2,1,0:T(8,128)S(1)} %get-tuple-element.115.b_ref.x_ref, bf16[44,2,128,128]{3,2,1,0:T(8,128)(2,1)S(1)} %get-tuple-element.74.refs_4_.split_ref.refs_2_.refs_6_, ...), custom_call_target="tpu_custom_call", output_to_operand_aliasing={{}: (4, {})} | custom-call | tf_op jit(solution)/shard_map/own/pallas_call | solution.py:504
  74.5 1.6 %collective-permute-start.28 = (f32[16,32,128]{2,1,0:T(8,128)S(1)}, f32[16,32,128]{2,1,0:T(8,128)S(1)}, u32[]{:S(2)}, u32[]{:S(2)}) collective-permute-start(f32[16,32,128]{2,1,0:T(8,128)S(1)} %add.53), channel_id=1, source_target_pairs={{0,2},{1,3},{2,0},{3,1},{4,6},{5,7},{6,4},{7,5},{8,10},{9,11},{10,... | collective-permute-start | bytes 786440 | tf_op jit(solution)/shard_map/ppermute | solution.py:489
  76.0 2.5 %collective-permute-done.21.refs_1_ = f32[8,32,128]{2,1,0:T(8,128)S(1)} collective-permute-done((f32[8,32,128]{2,1,0:T(8,128)S(1)}, f32[8,32,128]{2,1,0:T(8,128)S(1)}, u32[]{:S(2)}, u32[]{:S(2)}) %collective-permute-start.21) | collective-permute-done | bytes 131104 | tf_op jit(solution)/shard_map/ppermute | solution.py:119
  79.5 5.6 %collective-permute-done.25 = f32[64,128]{1,0:T(8,128)S(1)} collective-permute-done((f32[64,128]{1,0:T(8,128)S(1)}, f32[64,128]{1,0:T(8,128)S(1)}, u32[]{:S(2)}, u32[]{:S(2)}) %collective-permute-start.25) | collective-permute-done | bytes 32800 | tf_op jit(solution)/shard_map/ppermute | solution.py:149
  87.8 1.6 %collective-permute-start.27 = (f32[16,32,128]{2,1,0:T(8,128)S(1)}, f32[16,32,128]{2,1,0:T(8,128)S(1)}, u32[]{:S(2)}, u32[]{:S(2)}) collective-permute-start(f32[16,32,128]{2,1,0:T(8,128)S(1)} %add.55), channel_id=1, source_target_pairs={{0,2},{1,3},{2,0},{3,1},{4,6},{5,7},{6,4},{7,5},{8,10},{9,11},{10,... | collective-permute-start | bytes 786440 | tf_op jit(solution)/shard_map/ppermute | solution.py:489
  89.4 3.9 %second.1 = (f32[64,64]{1,0:T(8,128)S(1)}, f32[64,64]{1,0:T(8,128)S(1)}, f32[128,192]{1,0:T(8,128)S(1)}, f32[64,64]{1,0:T(8,128)S(1)}) custom-call(f32[64,128]{1,0:T(8,128)S(1)} %add.54.gram_ref, f32[64,64]{1,0:T(8,128)S(1)} %first.1.inverse_ref), custom_call_target="tpu_custom_call" | custom-call | tf_op jit(solution)/shard_map/second/pallas_call | solution.py:579
  93.3 1.7 %blend.2 = (f32[16,64,128]{2,1,0:T(8,128)S(1)}, f32[16,64,128]{2,1,0:T(8,128)S(1)}, f32[64,64]{1,0:T(8,128)S(1)}) custom-call(s32[4]{0:T(128)S(1)} %pad_add_fusion.place_ref, f32[32,64,128]{2,1,0:T(8,128)S(1)} %get-tuple-element.117.refs_3_.x_ref, f32[32,32,128]{2,1,0:T(8,128)S(1)} %get-tuple-element.102.x_ref.a_ref, ...), custom_call_target="tpu_custom_call" | custom-call | tf_op jit(solution)/shard_map/blend/pallas_call | solution.py:423
  95.1 1.7 %blend.3 = (f32[16,64,128]{2,1,0:T(8,128)S(1)}, f32[16,64,128]{2,1,0:T(8,128)S(1)}, f32[64,64]{1,0:T(8,128)S(1)}) custom-call(s32[4]{0:T(128)S(1)} %pad_add_fusion.place_ref, f32[32,64,128]{2,1,0:T(8,128)S(1)} %get-tuple-element.117.refs_3_.x_ref, f32[32,32,128]{2,1,0:T(8,128)S(1)} %get-tuple-element.102.x_ref.a_ref, ...), custom_call_target="tpu_custom_call" | custom-call | tf_op jit(solution)/shard_map/blend/pallas_call | solution.py:423
  98.4 2.0 %third.1 = (f32[32,64,128]{2,1,0:T(8,128)S(1)}, f32[72,128]{1,0:T(8,128)S(1)}) custom-call(s32[4]{0:T(128)S(1)} %pad_add_fusion.place_ref, f32[16,32,128]{2,1,0:T(8,128)S(1)} %add.57.mine_ref, f32[16,32,128]{2,1,0:T(8,128)S(1)} %collective-permute-done.30.other_ref, f32[64,64]{1,0:T(8,128)S(1)} %get-tuple-element.132.gain_ref, ...), custom_call_target="tpu_custom_call" | custom-call | tf_op jit(solution)/shard_map/third/pallas_call | solution.py:586
  101.4 3.1 %collective-permute-done.31 = f32[72,128]{1,0:T(8,128)S(1)} collective-permute-done((f32[72,128]{1,0:T(8,128)S(1)}, f32[72,128]{1,0:T(8,128)S(1)}, u32[]{:S(2)}, u32[]{:S(2)}) %collective-permute-start.31) | collective-permute-done | bytes 36896 | tf_op jit(solution)/shard_map/ppermute | solution.py:140
  104.5 4.9 %collective-permute-done.32 = f32[72,128]{1,0:T(8,128)S(1)} collective-permute-done((f32[72,128]{1,0:T(8,128)S(1)}, f32[72,128]{1,0:T(8,128)S(1)}, u32[]{:S(2)}, u32[]{:S(2)}) %collective-permute-start.32) | collective-permute-done | bytes 36896 | tf_op jit(solution)/shard_map/ppermute | solution.py:149
  109.3 3.7 %fourth.1 = (f32[64,64]{1,0:T(8,128)S(1)}, f32[64,64]{1,0:T(8,128)S(1)}, f32[64,128]{1,0:T(8,128)S(1)}) custom-call(f32[72,128]{1,0:T(8,128)S(1)} %add.59.gram_ref), custom_call_target="tpu_custom_call" | custom-call | tf_op jit(solution)/shard_map/fourth/pallas_call | solution.py:594
  113.0 1.9 %last.1 = (f32[32,64,128]{2,1,0:T(8,128)}, f32[4,64,64]{2,1,0:T(8,128)}) custom-call(f32[32,64,128]{2,1,0:T(8,128)S(1)} %get-tuple-element.137.w_ref, f32[16,64,128]{2,1,0:T(8,128)S(1)} %get-tuple-element.135.refs_2_.low_ref, f32[16,64,128]{2,1,0:T(8,128)S(1)} %get-tuple-element.136.refs_3_.high_ref, f32[64,128]{1,0:T(8,128)S(1)} %get-tuple-element.139.coef_ref, ...), custom_call_target="tpu_custom_call" | custom-call | tf_op jit(solution)/shard_map/last/pallas_call | solution.py:597
  (86 shorter events, 30.6 us)
Async XLA Ops:
  0.6 8.8 %collective-permute-start = (s32[1,1,44]{2,1,0:T(1,128)}, s32[1,1,44]{2,1,0:T(1,128)S(1)}, u32[]{:S(2)}, u32[]{:S(2)}) collective-permute-start(s32[1,1,44]{2,1,0:T(1,128)} %cols_ref.5), channel_id=1, source_target_pairs={{0,8},{4,12},{8,0},{12,4},{1,9},{5,13},{9,1},{13,5},{2,10},{6,14},... | collective-permute-start | bytes 536 | tf_op jit(solution)/shard_map/ppermute | solution.py:119
  4.8 4.7 %collective-permute-start.1 = (s32[1,1,44]{2,1,0:T(1,128)}, s32[1,1,44]{2,1,0:T(1,128)S(1)}, u32[]{:S(2)}, u32[]{:S(2)}) collective-permute-start(s32[1,1,44]{2,1,0:T(1,128)} %cols_ref.5), channel_id=1, source_target_pairs={{0,4},{8,12},{4,0},{12,8},{1,5},{9,13},{5,1},{13,9},{2,6},{10,14},... | collective-permute-start | bytes 536 | tf_op jit(solution)/shard_map/ppermute | solution.py:119
  6.3 5.5 %collective-permute-start.2 = (s32[1,1,44]{2,1,0:T(1,128)}, s32[1,1,44]{2,1,0:T(1,128)S(1)}, u32[]{:S(2)}, u32[]{:S(2)}) collective-permute-start(s32[1,1,44]{2,1,0:T(1,128)} %cols_ref.5), channel_id=1, source_target_pairs={{4,8},{0,12},{8,4},{12,0},{5,9},{1,13},{9,5},{13,1},{6,10},{2,14},... | collective-permute-start | bytes 536 | tf_op jit(solution)/shard_map/ppermute | solution.py:119
  13.3 6.5 %collective-permute-start.5 = (f32[8,32,128]{2,1,0:T(8,128)S(1)}, f32[8,32,128]{2,1,0:T(8,128)S(1)}, u32[]{:S(2)}, u32[]{:S(2)}) collective-permute-start(f32[8,32,128]{2,1,0:T(8,128)S(1)} %get-tuple-element.78), channel_id=1, source_target_pairs={{0,4},{8,12},{4,0},{12,8},{1,5},{9,13},{5,1},{13,9},{2,6},{10,14},... | collective-permute-start | bytes 393224 | tf_op jit(solution)/shard_map/ppermute | solution.py:119
  13.3 17.5 %collective-permute-start.3 = (f32[8,32,128]{2,1,0:T(8,128)S(1)}, f32[8,32,128]{2,1,0:T(8,128)S(1)}, u32[]{:S(2)}, u32[]{:S(2)}) collective-permute-start(f32[8,32,128]{2,1,0:T(8,128)S(1)} %get-tuple-element.76), channel_id=1, source_target_pairs={{0,8},{4,12},{8,0},{12,4},{1,9},{5,13},{9,1},{13,5},{2,10},{6,14},... | collective-permute-start | bytes 393224 | tf_op jit(solution)/shard_map/ppermute | solution.py:119
  14.6 8.4 %collective-permute-start.4 = (f32[8,32,128]{2,1,0:T(8,128)S(1)}, f32[8,32,128]{2,1,0:T(8,128)S(1)}, u32[]{:S(2)}, u32[]{:S(2)}) collective-permute-start(f32[8,32,128]{2,1,0:T(8,128)S(1)} %get-tuple-element.77), channel_id=1, source_target_pairs={{4,8},{0,12},{8,4},{12,0},{5,9},{1,13},{9,5},{13,1},{6,10},{2,14},... | collective-permute-start | bytes 393224 | tf_op jit(solution)/shard_map/ppermute | solution.py:119
  21.2 8.4 %collective-permute-start.6 = (f32[64,64]{1,0:T(8,128)S(1)}, f32[64,64]{1,0:T(8,128)S(1)}, u32[]{:S(2)}, u32[]{:S(2)}) collective-permute-start(f32[64,64]{1,0:T(8,128)S(1)} %gram.1), channel_id=1, source_target_pairs={{0,4},{4,0},{8,12},{12,8},{1,5},{5,1},{9,13},{13,9},{2,6},{6,2},{1... | collective-permute-start | bytes 49160 | tf_op jit(solution)/shard_map/ppermute | solution.py:140
  23.9 16.2 %collective-permute-start.8 = (f32[8,32,128]{2,1,0:T(8,128)S(1)}, f32[8,32,128]{2,1,0:T(8,128)S(1)}, u32[]{:S(2)}, u32[]{:S(2)}) collective-permute-start(f32[8,32,128]{2,1,0:T(8,128)S(1)} %get-tuple-element.91), channel_id=1, source_target_pairs={{4,8},{0,12},{8,4},{12,0},{5,9},{1,13},{9,5},{13,1},{6,10},{2,14},... | collective-permute-start | bytes 393224 | tf_op jit(solution)/shard_map/ppermute | solution.py:119
  25.8 7.7 %collective-permute-start.9 = (f32[8,32,128]{2,1,0:T(8,128)S(1)}, f32[8,32,128]{2,1,0:T(8,128)S(1)}, u32[]{:S(2)}, u32[]{:S(2)}) collective-permute-start(f32[8,32,128]{2,1,0:T(8,128)S(1)} %get-tuple-element.92), channel_id=1, source_target_pairs={{0,4},{8,12},{4,0},{12,8},{1,5},{9,13},{5,1},{13,9},{2,6},{10,14},... | collective-permute-start | bytes 393224 | tf_op jit(solution)/shard_map/ppermute | solution.py:119
  29.6 7.5 %collective-permute-start.10 = (f32[64,64]{1,0:T(8,128)S(1)}, f32[64,64]{1,0:T(8,128)S(1)}, u32[]{:S(2)}, u32[]{:S(2)}) collective-permute-start(f32[64,64]{1,0:T(8,128)S(1)} %add.46), channel_id=1, source_target_pairs={{0,8},{4,12},{8,0},{12,4},{1,9},{5,13},{9,1},{13,5},{2,10},{6,14},... | collective-permute-start | bytes 49160 | tf_op jit(solution)/shard_map/ppermute | solution.py:149
  31.9 11.6 %collective-permute-start.7 = (f32[8,32,128]{2,1,0:T(8,128)S(1)}, f32[8,32,128]{2,1,0:T(8,128)S(1)}, u32[]{:S(2)}, u32[]{:S(2)}) collective-permute-start(f32[8,32,128]{2,1,0:T(8,128)S(1)} %get-tuple-element.90), channel_id=1, source_target_pairs={{0,8},{4,12},{8,0},{12,4},{1,9},{5,13},{9,1},{13,5},{2,10},{6,14},... | collective-permute-start | bytes 393224 | tf_op jit(solution)/shard_map/ppermute | solution.py:119
  35.0 8.4 %collective-permute-start.13 = (f32[16,32,128]{2,1,0:T(8,128)S(1)}, f32[16,32,128]{2,1,0:T(8,128)S(1)}, u32[]{:S(2)}, u32[]{:S(2)}) collective-permute-start(f32[16,32,128]{2,1,0:T(8,128)S(1)} %add.47), channel_id=1, source_target_pairs={{0,2},{1,3},{2,0},{3,1},{4,6},{5,7},{6,4},{7,5},{8,10},{9,11},{10,... | collective-permute-start | bytes 786440 | tf_op jit(solution)/shard_map/ppermute | solution.py:489
  43.4 1.7 %collective-permute-start.14 = (f32[16,32,128]{2,1,0:T(8,128)S(1)}, f32[16,32,128]{2,1,0:T(8,128)S(1)}, u32[]{:S(2)}, u32[]{:S(2)}) collective-permute-start(f32[16,32,128]{2,1,0:T(8,128)S(1)} %add.49.refs_3_), channel_id=1, source_target_pairs={{0,1},{1,0},{2,3},{3,2},{4,5},{5,4},{6,7},{7,6},{8,9},{9,8},{10,11... | collective-permute-start | bytes 786440 | tf_op jit(solution)/shard_map/ppermute | solution.py:550
  44.5 3.0 %collective-permute-start.12 = (f32[16,32,128]{2,1,0:T(8,128)S(1)}, f32[16,32,128]{2,1,0:T(8,128)S(1)}, u32[]{:S(2)}, u32[]{:S(2)}) collective-permute-start(f32[16,32,128]{2,1,0:T(8,128)S(1)} %get-tuple-element.99), channel_id=1, source_target_pairs={{0,1},{1,0},{2,3},{3,2},{4,5},{5,4},{6,7},{7,6},{8,9},{9,8},{10,11... | collective-permute-start | bytes 786440 | tf_op jit(solution)/shard_map/ppermute | solution.py:554
  46.6 12.0 %collective-permute-start.17 = (f32[8,32,128]{2,1,0:T(8,128)S(1)}, f32[8,32,128]{2,1,0:T(8,128)S(1)}, u32[]{:S(2)}, u32[]{:S(2)}) collective-permute-start(f32[8,32,128]{2,1,0:T(8,128)S(1)} %get-tuple-element.105), channel_id=1, source_target_pairs={{0,8},{4,12},{8,0},{12,4},{1,9},{5,13},{9,1},{13,5},{2,10},{6,14},... | collective-permute-start | bytes 393224 | tf_op jit(solution)/shard_map/ppermute | solution.py:119
  47.6 14.7 %collective-permute-start.15 = (f32[16,32,128]{2,1,0:T(8,128)S(1)}, f32[16,32,128]{2,1,0:T(8,128)S(1)}, u32[]{:S(2)}, u32[]{:S(2)}) collective-permute-start(f32[16,32,128]{2,1,0:T(8,128)S(1)} %add.50), channel_id=1, source_target_pairs={{0,2},{1,3},{2,0},{3,1},{4,6},{5,7},{6,4},{7,5},{8,10},{9,11},{10,... | collective-permute-start | bytes 786440 | tf_op jit(solution)/shard_map/ppermute | solution.py:489
  49.1 12.1 %collective-permute-start.16 = (f32[8,32,128]{2,1,0:T(8,128)S(1)}, f32[8,32,128]{2,1,0:T(8,128)S(1)}, u32[]{:S(2)}, u32[]{:S(2)}) collective-permute-start(f32[8,32,128]{2,1,0:T(8,128)S(1)} %get-tuple-element.104), channel_id=1, source_target_pairs={{4,8},{0,12},{8,4},{12,0},{5,9},{1,13},{9,5},{13,1},{6,10},{2,14},... | collective-permute-start | bytes 393224 | tf_op jit(solution)/shard_map/ppermute | solution.py:119
  51.0 11.4 %collective-permute-start.19 = (f32[8,32,128]{2,1,0:T(8,128)S(1)}, f32[8,32,128]{2,1,0:T(8,128)S(1)}, u32[]{:S(2)}, u32[]{:S(2)}) collective-permute-start(f32[8,32,128]{2,1,0:T(8,128)S(1)} %get-tuple-element.109), channel_id=1, source_target_pairs={{0,4},{8,12},{4,0},{12,8},{1,5},{9,13},{5,1},{13,9},{2,6},{10,14},... | collective-permute-start | bytes 393224 | tf_op jit(solution)/shard_map/ppermute | solution.py:119
  62.3 1.6 %collective-permute-start.18 = (f32[16,32,128]{2,1,0:T(8,128)S(1)}, f32[16,32,128]{2,1,0:T(8,128)S(1)}, u32[]{:S(2)}, u32[]{:S(2)}) collective-permute-start(f32[16,32,128]{2,1,0:T(8,128)S(1)} %add.51.refs_3_), channel_id=1, source_target_pairs={{0,1},{1,0},{2,3},{3,2},{4,5},{5,4},{6,7},{7,6},{8,9},{9,8},{10,11... | collective-permute-start | bytes 786440 | tf_op jit(solution)/shard_map/ppermute | solution.py:560
  65.5 7.9 %collective-permute-start.22 = (f32[8,32,128]{2,1,0:T(8,128)S(1)}, f32[8,32,128]{2,1,0:T(8,128)S(1)}, u32[]{:S(2)}, u32[]{:S(2)}) collective-permute-start(f32[8,32,128]{2,1,0:T(8,128)S(1)} %get-tuple-element.114), channel_id=1, source_target_pairs={{0,4},{8,12},{4,0},{12,8},{1,5},{9,13},{5,1},{13,9},{2,6},{10,14},... | collective-permute-start | bytes 393224 | tf_op jit(solution)/shard_map/ppermute | solution.py:119
  67.0 6.2 %collective-permute-start.23 = (f32[64,128]{1,0:T(8,128)S(1)}, f32[64,128]{1,0:T(8,128)S(1)}, u32[]{:S(2)}, u32[]{:S(2)}) collective-permute-start(f32[64,128]{1,0:T(8,128)S(1)} %cross.1), channel_id=1, source_target_pairs={{0,4},{4,0},{8,12},{12,8},{1,5},{5,1},{9,13},{13,9},{2,6},{6,2},{1... | collective-permute-start | bytes 98312 | tf_op jit(solution)/shard_map/ppermute | solution.py:140
  68.7 5.7 %collective-permute-start.24 = (f32[16,32,128]{2,1,0:T(8,128)S(1)}, f32[16,32,128]{2,1,0:T(8,128)S(1)}, u32[]{:S(2)}, u32[]{:S(2)}) collective-permute-start(f32[16,32,128]{2,1,0:T(8,128)S(1)} %get-tuple-element.119), channel_id=1, source_target_pairs={{0,1},{1,0},{2,3},{3,2},{4,5},{5,4},{6,7},{7,6},{8,9},{9,8},{10,11... | collective-permute-start | bytes 786440 | tf_op jit(solution)/shard_map/ppermute | solution.py:565
  68.7 16.4 %collective-permute-start.20 = (f32[8,32,128]{2,1,0:T(8,128)S(1)}, f32[8,32,128]{2,1,0:T(8,128)S(1)}, u32[]{:S(2)}, u32[]{:S(2)}) collective-permute-start(f32[8,32,128]{2,1,0:T(8,128)S(1)} %get-tuple-element.112), channel_id=1, source_target_pairs={{0,8},{4,12},{8,0},{12,4},{1,9},{5,13},{9,1},{13,5},{2,10},{6,14},... | collective-permute-start | bytes 393224 | tf_op jit(solution)/shard_map/ppermute | solution.py:119
  69.0 9.5 %collective-permute-start.21 = (f32[8,32,128]{2,1,0:T(8,128)S(1)}, f32[8,32,128]{2,1,0:T(8,128)S(1)}, u32[]{:S(2)}, u32[]{:S(2)}) collective-permute-start(f32[8,32,128]{2,1,0:T(8,128)S(1)} %get-tuple-element.113), channel_id=1, source_target_pairs={{4,8},{0,12},{8,4},{12,0},{5,9},{1,13},{9,5},{13,1},{6,10},{2,14},... | collective-permute-start | bytes 393224 | tf_op jit(solution)/shard_map/ppermute | solution.py:119
  73.2 12.0 %collective-permute-start.25 = (f32[64,128]{1,0:T(8,128)S(1)}, f32[64,128]{1,0:T(8,128)S(1)}, u32[]{:S(2)}, u32[]{:S(2)}) collective-permute-start(f32[64,128]{1,0:T(8,128)S(1)} %add.52), channel_id=1, source_target_pairs={{0,8},{4,12},{8,0},{12,4},{1,9},{5,13},{9,1},{13,5},{2,10},{6,14},... | collective-permute-start | bytes 98312 | tf_op jit(solution)/shard_map/ppermute | solution.py:149
  74.5 11.8 %collective-permute-start.28 = (f32[16,32,128]{2,1,0:T(8,128)S(1)}, f32[16,32,128]{2,1,0:T(8,128)S(1)}, u32[]{:S(2)}, u32[]{:S(2)}) collective-permute-start(f32[16,32,128]{2,1,0:T(8,128)S(1)} %add.53), channel_id=1, source_target_pairs={{0,2},{1,3},{2,0},{3,1},{4,6},{5,7},{6,4},{7,5},{8,10},{9,11},{10,... | collective-permute-start | bytes 786440 | tf_op jit(solution)/shard_map/ppermute | solution.py:489
  86.2 1.6 %collective-permute-start.26 = (f32[16,32,128]{2,1,0:T(8,128)S(1)}, f32[16,32,128]{2,1,0:T(8,128)S(1)}, u32[]{:S(2)}, u32[]{:S(2)}) collective-permute-start(f32[16,32,128]{2,1,0:T(8,128)S(1)} %get-tuple-element.125), channel_id=1, source_target_pairs={{0,1},{1,0},{2,3},{3,2},{4,5},{5,4},{6,7},{7,6},{8,9},{9,8},{10,11... | collective-permute-start | bytes 786440 | tf_op jit(solution)/shard_map/ppermute | solution.py:577
  86.4 7.0 %collective-permute-start.29 = (f32[16,32,128]{2,1,0:T(8,128)S(1)}, f32[16,32,128]{2,1,0:T(8,128)S(1)}, u32[]{:S(2)}, u32[]{:S(2)}) collective-permute-start(f32[16,32,128]{2,1,0:T(8,128)S(1)} %add.56.mine_ref), channel_id=1, source_target_pairs={{0,1},{1,0},{2,3},{3,2},{4,5},{5,4},{6,7},{7,6},{8,9},{9,8},{10,11... | collective-permute-start | bytes 786440 | tf_op jit(solution)/shard_map/ppermute | solution.py:574
  87.8 9.0 %collective-permute-start.27 = (f32[16,32,128]{2,1,0:T(8,128)S(1)}, f32[16,32,128]{2,1,0:T(8,128)S(1)}, u32[]{:S(2)}, u32[]{:S(2)}) collective-permute-start(f32[16,32,128]{2,1,0:T(8,128)S(1)} %add.55), channel_id=1, source_target_pairs={{0,2},{1,3},{2,0},{3,1},{4,6},{5,7},{6,4},{7,5},{8,10},{9,11},{10,... | collective-permute-start | bytes 786440 | tf_op jit(solution)/shard_map/ppermute | solution.py:489
  96.8 1.6 %collective-permute-start.30 = (f32[16,32,128]{2,1,0:T(8,128)S(1)}, f32[16,32,128]{2,1,0:T(8,128)S(1)}, u32[]{:S(2)}, u32[]{:S(2)}) collective-permute-start(f32[16,32,128]{2,1,0:T(8,128)S(1)} %add.57.mine_ref), channel_id=1, source_target_pairs={{0,1},{1,0},{2,3},{3,2},{4,5},{5,4},{6,7},{7,6},{8,9},{9,8},{10,11... | collective-permute-start | bytes 786440 | tf_op jit(solution)/shard_map/ppermute | solution.py:585
  100.4 4.0 %collective-permute-start.31 = (f32[72,128]{1,0:T(8,128)S(1)}, f32[72,128]{1,0:T(8,128)S(1)}, u32[]{:S(2)}, u32[]{:S(2)}) collective-permute-start(f32[72,128]{1,0:T(8,128)S(1)} %get-tuple-element.138), channel_id=1, source_target_pairs={{0,4},{4,0},{8,12},{12,8},{1,5},{5,1},{9,13},{13,9},{2,6},{6,2},{1... | collective-permute-start | bytes 110600 | tf_op jit(solution)/shard_map/ppermute | solution.py:140
  104.4 4.9 %collective-permute-start.32 = (f32[72,128]{1,0:T(8,128)S(1)}, f32[72,128]{1,0:T(8,128)S(1)}, u32[]{:S(2)}, u32[]{:S(2)}) collective-permute-start(f32[72,128]{1,0:T(8,128)S(1)} %add.58), channel_id=1, source_target_pairs={{0,8},{4,12},{8,0},{12,4},{1,9},{5,13},{9,1},{13,5},{2,10},{6,14},... | collective-permute-start | bytes 110600 | tf_op jit(solution)/shard_map/ppermute | solution.py:149
  (5 other events, 33.9 us)

commit v8 on v7

--- a/solution.py
+++ b/solution.py
@@ -227,13 +227,21 @@
     ).astype(jnp.int32)
 
     def own_sum(acc_refs, x_ref, split_ref, rows_ref, cols_ref):
-        for s in range(OWN_SLOTS):
-            i, j = rows_ref[0, 0, s], cols_ref[0, 0, s]
-            direct = tile_product(x_ref[j], split_ref, s, True)
-            mirror = tile_product(x_ref[i], split_ref, s, False)
-            for n, acc_ref in enumerate(acc_refs):
-                acc_ref[i] += direct[n * part : (n + 1) * part]
-                acc_ref[j] += mirror[n * part : (n + 1) * part]
+        batch = 4
+        for first in range(0, OWN_SLOTS, batch):
+            members = range(first, first + batch)
+            ends = [(rows_ref[0, 0, s], cols_ref[0, 0, s]) for s in members]
+            terms = [
+                (
+                    tile_product(x_ref[j], split_ref, s, True),
+                    tile_product(x_ref[i], split_ref, s, False),
+                )
+                for s, (i, j) in zip(members, ends)
+            ]
+            for (i, j), (direct, mirror) in zip(ends, terms):
+                for n, acc_ref in enumerate(acc_refs):
+                    acc_ref[i] += direct[n * part : (n + 1) * part]
+                    acc_ref[j] += mirror[n * part : (n + 1) * part]
 
     def prepare_body(x_hbm, diag_hbm, tiles_hbm, *refs):
         x_ref, split_ref, a_ref, b_ref, diag_ref, raw_ref, sem = refs
@@ -275,8 +283,11 @@
             @pl.when(role > 0)
             def _():
                 base = OWN_SLOTS + (role - 1) * CAP
-                for c in range(CAP):
-                    term = tile_product(x_ref[rows_ref[0, 0, base + c]], split_ref, base + c, False)
+                terms = [
+                    tile_product(x_ref[rows_ref[0, 0, base + c]], split_ref, base + c, False)
+                    for c in range(CAP)
+                ]
+                for c, term in enumerate(terms):
                     put(c, jnp.where(c < counts_ref[0, 0, role - 1], term, 0.0))
 
             @pl.when(role < 0)
@@ -316,8 +327,10 @@
             @pl.when(role > 0)
             def _():
                 base = OWN_SLOTS + (role - 1) * CAP
-                for c in range(CAP):
-                    term = tile_product(got_refs[n][c], split_ref, base + c, True)
+                terms = [
+                    tile_product(got_refs[n][c], split_ref, base + c, True) for c in range(CAP)
+                ]
+                for c, term in enumerate(terms):
                     acc_ref[rows_ref[0, 0, base + c]] += jnp.where(
                         c < counts_ref[0, 0, role - 1], term, 0.0
                     )
@@ -553,26 +566,26 @@
 
     core = lax.ppermute(give_b, "vec", swap)
     mine_b = keep_b + after(core, y_a)
-    acc_a = join(after(acc_a, mine_b), got_a, groups[2])
-    (acc_a,) = own(y_a, acc_a)
+    (acc_a,) = own(y_a, after(acc_a, mine_b))
+    acc_a = join(acc_a, got_a, groups[2])
     acc_a = join(acc_a, got_a, groups[1])
     mine_b = across(mine_b, acc_a)
     other_b = lax.ppermute(mine_b, "vec", swap)
     keep_a, give_a = join(acc_a, got_a, groups[0], last=True)
     y_b, acc_b, got_b = resend(mine_b, after(other_b, keep_a))
 
-    (gram,) = call(cross_body, [(width, 2 * width)], [VMEM] * 3, name="cross")(x, y_a, y_b)
     core = lax.ppermute(give_a, "vec", swap)
+    mine_a = keep_a + after(core, y_b)
+    (gram,) = call(cross_body, [(width, 2 * width)], [VMEM] * 3, name="cross")(x, y_a, after(y_b, mine_a))
     (acc_b,) = own(y_b, after(acc_b, gram))
-    acc_b = join(acc_b, got_b, groups[0])
-    mine_a = keep_a + after(core, acc_b)
     cross_gram = start_sum(gram, "res")
-    acc_b = join(after(acc_b, cross_gram, mine_a), got_b, groups[1])
+    acc_b = join(after(acc_b, cross_gram), got_b, groups[2])
+    acc_b = join(acc_b, got_b, groups[1])
     cross_gram = end_sum(cross_gram, "res", acc_b)
     acc_b = after(acc_b, cross_gram)
     mine_a = across(mine_a, acc_b)
     other_a = lax.ppermute(mine_a, "vec", swap)
-    keep_b, give_b = join(acc_b, got_b, groups[2], last=True)
+    keep_b, give_b = join(acc_b, got_b, groups[0], last=True)
 
     core = lax.ppermute(give_b, "vec", swap)
     mine_b = keep_b + core

time: 115 us -> 111 us (0.965)
  waiting for transfers between devices: 33.4 us -> 27.1 us
  starting transfers between devices: 35.9 us -> 38.1 us
    ppermute x3, waiting for transfers between devices: 11.1 us -> 5.53 us  [end_sum(): got = lax.ppermute(block, axis, [(i, i ^ step) for i in range(size)])]
    ppermute x15, starting transfers between devices: 24 us -> 28 us  [exchange(): lax.ppermute(block, axis, [(a, b) for a, b in pairs] + [(b, a) for a, b i...]
  transfers between devices with their start and end apart: 33 -> 33, of which waited for: 14 -> 14; matrix products, arithmetic and copies ran while one was open for 1% -> 1% of each run, Pallas kernels for 29% -> 31%
where the time goes in v8:
time: 111 us
  Pallas kernels  43.5 us (39%)
  starting transfers between devices  38.1 us (34%)
  waiting for transfers between devices  27.1 us (24%)
    ppermute x15, starting transfers between devices, exchange(): lax.ppermute(block, axis, [(a, b) for a, b in pairs] + [(b, a) for a, b i...  28 us
    ppermute x15, waiting for transfers between devices, exchange(): lax.ppermute(block, axis, [(a, b) for a, b in pairs] + [(b, a) for a, b i...  13.6 us
    pallas_call x12, Pallas kernels, join(): call(body, [halfchunk] * 2 if last else [chunk], [SMEM] * (3 + size) + [V...  11.7 us
    ppermute x3, waiting for transfers between devices, end_sum(): got = lax.ppermute(block, axis, [(i, i ^ step) for i in range(size)])  5.53 us
    pallas_call x3, Pallas kernels, own(): call(own_body, [chunk] * len(accs), [SMEM] * 2 + [VMEM] * (2 + len(accs))...  5.46 us
    ppermute x4, starting transfers between devices, across(): got = lax.ppermute(mine, 'vec', [(i, i ^ step) for i in range(lanes)])  5.32 us
    pallas_call x1, Pallas kernels, local(): call(second_body, [square, square, (2 * width, 3 * width), square], [VMEM...  3.94 us
    pallas_call x1, Pallas kernels, local(): call(fourth_body, [square, square, (width, 2 * width)], [VMEM], name='fou...  3.7 us
  transfers between devices with their start and end apart: 33, of which 14 were waited for; matrix products, arithmetic and copies ran while one was open for 1% of the time, Pallas kernels for 31%

profile of v8, /device:TPU:0, one launch (start us, length us, event | category | flops | bytes accessed | tf_op | source)
XLA Modules:
  0.0 110.8 jit_solution(13740127498957217891)
XLA Ops:
  0.6 4.1 %collective-permute-start.2 = (s32[1,1,44]{2,1,0:T(1,128)}, s32[1,1,44]{2,1,0:T(1,128)S(1)}, u32[]{:S(2)}, u32[]{:S(2)}) collective-permute-start(s32[1,1,44]{2,1,0:T(1,128)} %cols_ref.5), channel_id=1, source_target_pairs={{0,8},{4,12},{8,0},{12,4},{1,9},{5,13},{9,1},{13,5},{2,10},{6,14},... | collective-permute-start | bytes 536 | tf_op jit(solution)/shard_map/ppermute | solution.py:119
  7.1 2.3 %prepare.1 = (f32[32,64,128]{2,1,0:T(8,128)S(1)}, bf16[44,2,128,128]{3,2,1,0:T(8,128)(2,1)S(1)}, f32[32,32,128]{2,1,0:T(8,128)S(1)}, f32[32,32,128]{2,1,0:T(8,128)S(1)}) custom-call(f32[32,64,128]{2,1,0:T(8,128)} %x_hbm.1, f32[32,128]{1,0:T(8,128)} %refs_5_.3, f32[1,1,44,128,128]{4,3,2,1,0:T(8,128)} %tiles_hbm.1), custom_call_target="tpu_custom_call" | custom-call | tf_op jit(solution)/shard_map/prepare/pallas_call | solution.py:526
  10.2 1.4 %send.1 = (f32[8,32,128]{2,1,0:T(8,128)S(1)}, f32[8,32,128]{2,1,0:T(8,128)S(1)}, f32[8,32,128]{2,1,0:T(8,128)S(1)}, f32[8,32,128]{2,1,0:T(8,128)S(1)}, f32[8,32,...) custom-call(s32[4]{0:T(128)S(1)} %pad_add_fusion.place_ref, s32[1,1,44]{2,1,0:T(1,128)S(1)} %copy-done.1, ...), custom_call_target="tpu_custom_call" | custom-call | tf_op jit(solution)/shard_map/send/pallas_call | solution.py:537
  13.7 2.4 %collective-permute-start.4 = (f32[8,32,128]{2,1,0:T(8,128)S(1)}, f32[8,32,128]{2,1,0:T(8,128)S(1)}, u32[]{:S(2)}, u32[]{:S(2)}) collective-permute-start(f32[8,32,128]{2,1,0:T(8,128)S(1)} %get-tuple-element.78), channel_id=1, source_target_pairs={{4,8},{0,12},{8,4},{12,0},{5,9},{1,13},{9,5},{13,1},{6,10},{2,14},... | collective-permute-start | bytes 393224 | tf_op jit(solution)/shard_map/ppermute | solution.py:119
  16.1 2.0 %own.3 = (f32[32,32,128]{2,1,0:T(8,128)S(1)}, f32[32,32,128]{2,1,0:T(8,128)S(1)}) custom-call(s32[1,1,44]{2,1,0:T(1,128)S(1)} %copy-done.1, s32[1,1,44]{2,1,0:T(1,128)S(1)} %copy-done.2, f32[32,64,128]{2,1,0:T(8,128)S(1)} %get-tuple-element.118.refs_3_.x_ref, ...), custom_call_target="tpu_custom_call", output_to_operand_aliasing={{0}: (4, {}), {1}: (5, {})} | custom-call | tf_op jit(solution)/shard_map/own/pallas_call | solution.py:517
  20.2 2.9 %collective-permute-done.4.refs_1_ = f32[8,32,128]{2,1,0:T(8,128)S(1)} collective-permute-done((f32[8,32,128]{2,1,0:T(8,128)S(1)}, f32[8,32,128]{2,1,0:T(8,128)S(1)}, u32[]{:S(2)}, u32[]{:S(2)}) %collective-permute-start.4) | collective-permute-done | bytes 131104 | tf_op jit(solution)/shard_map/ppermute | solution.py:119
  24.1 1.4 %collective-permute-start.8 = (f32[8,32,128]{2,1,0:T(8,128)S(1)}, f32[8,32,128]{2,1,0:T(8,128)S(1)}, u32[]{:S(2)}, u32[]{:S(2)}) collective-permute-start(f32[8,32,128]{2,1,0:T(8,128)S(1)} %get-tuple-element.92), channel_id=1, source_target_pairs={{4,8},{0,12},{8,4},{12,0},{5,9},{1,13},{9,5},{13,1},{6,10},{2,14},... | collective-permute-start | bytes 393224 | tf_op jit(solution)/shard_map/ppermute | solution.py:119
  25.4 4.5 %collective-permute-start.9 = (f32[8,32,128]{2,1,0:T(8,128)S(1)}, f32[8,32,128]{2,1,0:T(8,128)S(1)}, u32[]{:S(2)}, u32[]{:S(2)}) collective-permute-start(f32[8,32,128]{2,1,0:T(8,128)S(1)} %get-tuple-element.93), channel_id=1, source_target_pairs={{0,4},{8,12},{4,0},{12,8},{1,5},{9,13},{5,1},{13,9},{2,6},{10,14},... | collective-permute-start | bytes 393224 | tf_op jit(solution)/shard_map/ppermute | solution.py:119
  31.1 2.6 %collective-permute-start.7 = (f32[8,32,128]{2,1,0:T(8,128)S(1)}, f32[8,32,128]{2,1,0:T(8,128)S(1)}, u32[]{:S(2)}, u32[]{:S(2)}) collective-permute-start(f32[8,32,128]{2,1,0:T(8,128)S(1)} %get-tuple-element.91), channel_id=1, source_target_pairs={{0,8},{4,12},{8,0},{12,4},{1,9},{5,13},{9,1},{13,5},{2,10},{6,14},... | collective-permute-start | bytes 393224 | tf_op jit(solution)/shard_map/ppermute | solution.py:119
  35.3 1.6 %collective-permute-start.13 = (f32[16,32,128]{2,1,0:T(8,128)S(1)}, f32[16,32,128]{2,1,0:T(8,128)S(1)}, u32[]{:S(2)}, u32[]{:S(2)}) collective-permute-start(f32[16,32,128]{2,1,0:T(8,128)S(1)} %add.47), channel_id=1, source_target_pairs={{0,2},{1,3},{2,0},{3,1},{4,6},{5,7},{6,4},{7,5},{8,10},{9,11},{10,... | collective-permute-start | bytes 786440 | tf_op jit(solution)/shard_map/ppermute | solution.py:502
  36.8 1.6 %collective-permute-done.10 = f32[64,64]{1,0:T(8,128)S(1)} collective-permute-done((f32[64,64]{1,0:T(8,128)S(1)}, f32[64,64]{1,0:T(8,128)S(1)}, u32[]{:S(2)}, u32[]{:S(2)}) %collective-permute-start.10) | collective-permute-done | bytes 16416 | tf_op jit(solution)/shard_map/ppermute | solution.py:149
  38.4 3.0 %first.1.inverse_ref = f32[64,64]{1,0:T(8,128)S(1)} custom-call(f32[64,64]{1,0:T(8,128)S(1)} %add.48.gram_ref), custom_call_target="tpu_custom_call" | custom-call | tf_op jit(solution)/shard_map/first/pallas_call | solution.py:560
  45.4 1.4 %resend.2 = (f32[32,32,128]{2,1,0:T(8,128)S(1)}, f32[32,32,128]{2,1,0:T(8,128)S(1)}, f32[8,32,128]{2,1,0:T(8,128)S(1)}, f32[8,32,128]{2,1,0:T(8,128)S(1)}, f32[8,32,128]{2,1,0:T(8,128)S(1)}) custom-call(s32[4]{0:T(128)S(1)} %pad_add_fusion.place_ref, s32[1,1,44]{2,1,0:T(1,128)S(1)} %copy-done.1, s32[1,1,3]{2,1,0:T(1,128)S(1)} %copy-done.3, ...), custom_call_target="tpu_custom_call" | custom-call | tf_op jit(solution)/shard_map/resend/pallas_call | solution.py:508
  47.0 1.6 %collective-permute-start.15 = (f32[16,32,128]{2,1,0:T(8,128)S(1)}, f32[16,32,128]{2,1,0:T(8,128)S(1)}, u32[]{:S(2)}, u32[]{:S(2)}) collective-permute-start(f32[16,32,128]{2,1,0:T(8,128)S(1)} %add.50), channel_id=1, source_target_pairs={{0,2},{1,3},{2,0},{3,1},{4,6},{5,7},{6,4},{7,5},{8,10},{9,11},{10,... | collective-permute-start | bytes 786440 | tf_op jit(solution)/shard_map/ppermute | solution.py:502
  48.5 1.7 %own.4.refs_3_ = f32[32,32,128]{2,1,0:T(8,128)S(1)} custom-call(s32[1,1,44]{2,1,0:T(1,128)S(1)} %copy-done.1, s32[1,1,44]{2,1,0:T(1,128)S(1)} %copy-done.2, f32[32,32,128]{2,1,0:T(8,128)S(1)} %get-tuple-element.103.x_ref.a_ref, bf16[44,2,128,128]{3,2,1,0:T(8,128)(2,1)S(1)} %get-tuple-element.75.refs_4_.split_ref.refs_2_.refs_6_, ...), custom_call_target="tpu_custom_call", output_to_operand_aliasing={{}: (4, {})} | custom-call | tf_op jit(solution)/shard_map/own/pallas_call | solution.py:517
  50.3 2.2 %collective-permute-start.16 = (f32[8,32,128]{2,1,0:T(8,128)S(1)}, f32[8,32,128]{2,1,0:T(8,128)S(1)}, u32[]{:S(2)}, u32[]{:S(2)}) collective-permute-start(f32[8,32,128]{2,1,0:T(8,128)S(1)} %get-tuple-element.105), channel_id=1, source_target_pairs={{4,8},{0,12},{8,4},{12,0},{5,9},{1,13},{9,5},{13,1},{6,10},{2,14},... | collective-permute-start | bytes 393224 | tf_op jit(solution)/shard_map/ppermute | solution.py:119
  53.8 4.1 %collective-permute-done.17.refs_1_ = f32[8,32,128]{2,1,0:T(8,128)S(1)} collective-permute-done((f32[8,32,128]{2,1,0:T(8,128)S(1)}, f32[8,32,128]{2,1,0:T(8,128)S(1)}, u32[]{:S(2)}, u32[]{:S(2)}) %collective-permute-start.17) | collective-permute-done | bytes 131104 | tf_op jit(solution)/shard_map/ppermute | solution.py:119
  62.0 1.6 %resend.3 = (f32[32,32,128]{2,1,0:T(8,128)S(1)}, f32[32,32,128]{2,1,0:T(8,128)S(1)}, f32[8,32,128]{2,1,0:T(8,128)S(1)}, f32[8,32,128]{2,1,0:T(8,128)S(1)}, f32[8,32,128]{2,1,0:T(8,128)S(1)}) custom-call(s32[4]{0:T(128)S(1)} %pad_add_fusion.place_ref, s32[1,1,44]{2,1,0:T(1,128)S(1)} %copy-done.1, s32[1,1,3]{2,1,0:T(1,128)S(1)} %copy-done.3, ...), custom_call_target="tpu_custom_call" | custom-call | tf_op jit(solution)/shard_map/resend/pallas_call | solution.py:508
  66.8 1.5 %collective-permute-start.28 = (f32[16,32,128]{2,1,0:T(8,128)S(1)}, f32[16,32,128]{2,1,0:T(8,128)S(1)}, u32[]{:S(2)}, u32[]{:S(2)}) collective-permute-start(f32[16,32,128]{2,1,0:T(8,128)S(1)} %add.52), channel_id=1, source_target_pairs={{0,2},{1,3},{2,0},{3,1},{4,6},{5,7},{6,4},{7,5},{8,10},{9,11},{10,... | collective-permute-start | bytes 786440 | tf_op jit(solution)/shard_map/ppermute | solution.py:502
  68.2 1.7 %own.5.refs_3_ = f32[32,32,128]{2,1,0:T(8,128)S(1)} custom-call(s32[1,1,44]{2,1,0:T(1,128)S(1)} %copy-done.1, s32[1,1,44]{2,1,0:T(1,128)S(1)} %copy-done.2, f32[32,32,128]{2,1,0:T(8,128)S(1)} %get-tuple-element.121.b_ref.x_ref, bf16[44,2,128,128]{3,2,1,0:T(8,128)(2,1)S(1)} %get-tuple-element.75.refs_4_.split_ref.refs_2_.refs_6_, ...), custom_call_target="tpu_custom_call", output_to_operand_aliasing={{}: (4, {})} | custom-call | tf_op jit(solution)/shard_map/own/pallas_call | solution.py:517
  70.0 1.5 %collective-permute-start.20 = (f32[8,32,128]{2,1,0:T(8,128)S(1)}, f32[8,32,128]{2,1,0:T(8,128)S(1)}, u32[]{:S(2)}, u32[]{:S(2)}) collective-permute-start(f32[8,32,128]{2,1,0:T(8,128)S(1)} %get-tuple-element.113), channel_id=1, source_target_pairs={{0,4},{8,12},{4,0},{12,8},{1,5},{9,13},{5,1},{13,9},{2,6},{10,14},... | collective-permute-start | bytes 393224 | tf_op jit(solution)/shard_map/ppermute | solution.py:119
  71.5 2.9 %collective-permute-start.21 = (f32[8,32,128]{2,1,0:T(8,128)S(1)}, f32[8,32,128]{2,1,0:T(8,128)S(1)}, u32[]{:S(2)}, u32[]{:S(2)}) collective-permute-start(f32[8,32,128]{2,1,0:T(8,128)S(1)} %get-tuple-element.114), channel_id=1, source_target_pairs={{4,8},{0,12},{8,4},{12,0},{5,9},{1,13},{9,5},{13,1},{6,10},{2,14},... | collective-permute-start | bytes 393224 | tf_op jit(solution)/shard_map/ppermute | solution.py:119
  75.5 4.8 %collective-permute-done.21.refs_1_ = f32[8,32,128]{2,1,0:T(8,128)S(1)} collective-permute-done((f32[8,32,128]{2,1,0:T(8,128)S(1)}, f32[8,32,128]{2,1,0:T(8,128)S(1)}, u32[]{:S(2)}, u32[]{:S(2)}) %collective-permute-start.21) | collective-permute-done | bytes 131104 | tf_op jit(solution)/shard_map/ppermute | solution.py:119
  84.6 3.9 %second.1 = (f32[64,64]{1,0:T(8,128)S(1)}, f32[64,64]{1,0:T(8,128)S(1)}, f32[128,192]{1,0:T(8,128)S(1)}, f32[64,64]{1,0:T(8,128)S(1)}) custom-call(f32[64,128]{1,0:T(8,128)S(1)} %add.54.gram_ref, f32[64,64]{1,0:T(8,128)S(1)} %first.1.inverse_ref), custom_call_target="tpu_custom_call" | custom-call | tf_op jit(solution)/shard_map/second/pallas_call | solution.py:592
  88.6 1.7 %blend.3 = (f32[16,64,128]{2,1,0:T(8,128)S(1)}, f32[16,64,128]{2,1,0:T(8,128)S(1)}, f32[64,64]{1,0:T(8,128)S(1)}) custom-call(s32[4]{0:T(128)S(1)} %pad_add_fusion.place_ref, f32[32,64,128]{2,1,0:T(8,128)S(1)} %get-tuple-element.118.refs_3_.x_ref, f32[32,32,128]{2,1,0:T(8,128)S(1)} %get-tuple-element.103.x_ref.a_ref, ...), custom_call_target="tpu_custom_call" | custom-call | tf_op jit(solution)/shard_map/blend/pallas_call | solution.py:436
  90.3 1.7 %blend.2 = (f32[16,64,128]{2,1,0:T(8,128)S(1)}, f32[16,64,128]{2,1,0:T(8,128)S(1)}, f32[64,64]{1,0:T(8,128)S(1)}) custom-call(s32[4]{0:T(128)S(1)} %pad_add_fusion.place_ref, f32[32,64,128]{2,1,0:T(8,128)S(1)} %get-tuple-element.118.refs_3_.x_ref, f32[32,32,128]{2,1,0:T(8,128)S(1)} %get-tuple-element.103.x_ref.a_ref, ...), custom_call_target="tpu_custom_call" | custom-call | tf_op jit(solution)/shard_map/blend/pallas_call | solution.py:436
  92.4 1.5 %collective-permute-done.30.other_ref = f32[16,32,128]{2,1,0:T(8,128)S(1)} collective-permute-done((f32[16,32,128]{2,1,0:T(8,128)S(1)}, f32[16,32,128]{2,1,0:T(8,128)S(1)}, u32[]{:S(2)}, u32[]{:S(2)}) %collective-permute-start.30) | collective-permute-done | bytes 262176 | tf_op jit(solution)/shard_map/ppermute | solution.py:598
  94.0 2.0 %third.1 = (f32[32,64,128]{2,1,0:T(8,128)S(1)}, f32[72,128]{1,0:T(8,128)S(1)}) custom-call(s32[4]{0:T(128)S(1)} %pad_add_fusion.place_ref, f32[16,32,128]{2,1,0:T(8,128)S(1)} %add.57.mine_ref, f32[16,32,128]{2,1,0:T(8,128)S(1)} %collective-permute-done.30.other_ref, f32[64,64]{1,0:T(8,128)S(1)} %get-tuple-element.134.gain_ref, ...), custom_call_target="tpu_custom_call" | custom-call | tf_op jit(solution)/shard_map/third/pallas_call | solution.py:599
  96.6 3.4 %collective-permute-done.31 = f32[72,128]{1,0:T(8,128)S(1)} collective-permute-done((f32[72,128]{1,0:T(8,128)S(1)}, f32[72,128]{1,0:T(8,128)S(1)}, u32[]{:S(2)}, u32[]{:S(2)}) %collective-permute-start.31) | collective-permute-done | bytes 36896 | tf_op jit(solution)/shard_map/ppermute | solution.py:140
  101.3 3.9 %collective-permute-done.32 = f32[72,128]{1,0:T(8,128)S(1)} collective-permute-done((f32[72,128]{1,0:T(8,128)S(1)}, f32[72,128]{1,0:T(8,128)S(1)}, u32[]{:S(2)}, u32[]{:S(2)}) %collective-permute-start.32) | collective-permute-done | bytes 36896 | tf_op jit(solution)/shard_map/ppermute | solution.py:149
  105.2 3.7 %fourth.1 = (f32[64,64]{1,0:T(8,128)S(1)}, f32[64,64]{1,0:T(8,128)S(1)}, f32[64,128]{1,0:T(8,128)S(1)}) custom-call(f32[72,128]{1,0:T(8,128)S(1)} %add.59.gram_ref), custom_call_target="tpu_custom_call" | custom-call | tf_op jit(solution)/shard_map/fourth/pallas_call | solution.py:607
  109.0 1.9 %last.1 = (f32[32,64,128]{2,1,0:T(8,128)}, f32[4,64,64]{2,1,0:T(8,128)}) custom-call(f32[32,64,128]{2,1,0:T(8,128)S(1)} %get-tuple-element.139.w_ref, f32[16,64,128]{2,1,0:T(8,128)S(1)} %get-tuple-element.137.refs_2_.low_ref, f32[16,64,128]{2,1,0:T(8,128)S(1)} %get-tuple-element.138.refs_3_.high_ref, f32[64,128]{1,0:T(8,128)S(1)} %get-tuple-element.141.coef_ref, ...), custom_call_target="tpu_custom_call" | custom-call | tf_op jit(solution)/shard_map/last/pallas_call | solution.py:610
  (86 shorter events, 31.1 us)
Async XLA Ops:
  0.6 8.8 %collective-permute-start.2 = (s32[1,1,44]{2,1,0:T(1,128)}, s32[1,1,44]{2,1,0:T(1,128)S(1)}, u32[]{:S(2)}, u32[]{:S(2)}) collective-permute-start(s32[1,1,44]{2,1,0:T(1,128)} %cols_ref.5), channel_id=1, source_target_pairs={{0,8},{4,12},{8,0},{12,4},{1,9},{5,13},{9,1},{13,5},{2,10},{6,14},... | collective-permute-start | bytes 536 | tf_op jit(solution)/shard_map/ppermute | solution.py:119
  4.8 5.5 %collective-permute-start.1 = (s32[1,1,44]{2,1,0:T(1,128)}, s32[1,1,44]{2,1,0:T(1,128)S(1)}, u32[]{:S(2)}, u32[]{:S(2)}) collective-permute-start(s32[1,1,44]{2,1,0:T(1,128)} %cols_ref.5), channel_id=1, source_target_pairs={{4,8},{0,12},{8,4},{12,0},{5,9},{1,13},{9,5},{13,1},{6,10},{2,14},... | collective-permute-start | bytes 536 | tf_op jit(solution)/shard_map/ppermute | solution.py:119
  6.1 4.1 %collective-permute-start = (s32[1,1,44]{2,1,0:T(1,128)}, s32[1,1,44]{2,1,0:T(1,128)S(1)}, u32[]{:S(2)}, u32[]{:S(2)}) collective-permute-start(s32[1,1,44]{2,1,0:T(1,128)} %cols_ref.5), channel_id=1, source_target_pairs={{0,4},{8,12},{4,0},{12,8},{1,5},{9,13},{5,1},{13,9},{2,6},{10,14},... | collective-permute-start | bytes 536 | tf_op jit(solution)/shard_map/ppermute | solution.py:119
  11.7 6.5 %collective-permute-start.5 = (f32[8,32,128]{2,1,0:T(8,128)S(1)}, f32[8,32,128]{2,1,0:T(8,128)S(1)}, u32[]{:S(2)}, u32[]{:S(2)}) collective-permute-start(f32[8,32,128]{2,1,0:T(8,128)S(1)} %get-tuple-element.79), channel_id=1, source_target_pairs={{0,4},{8,12},{4,0},{12,8},{1,5},{9,13},{5,1},{13,9},{2,6},{10,14},... | collective-permute-start | bytes 393224 | tf_op jit(solution)/shard_map/ppermute | solution.py:119
  12.5 17.5 %collective-permute-start.3 = (f32[8,32,128]{2,1,0:T(8,128)S(1)}, f32[8,32,128]{2,1,0:T(8,128)S(1)}, u32[]{:S(2)}, u32[]{:S(2)}) collective-permute-start(f32[8,32,128]{2,1,0:T(8,128)S(1)} %get-tuple-element.77), channel_id=1, source_target_pairs={{0,8},{4,12},{8,0},{12,4},{1,9},{5,13},{9,1},{13,5},{2,10},{6,14},... | collective-permute-start | bytes 393224 | tf_op jit(solution)/shard_map/ppermute | solution.py:119
  13.7 9.4 %collective-permute-start.4 = (f32[8,32,128]{2,1,0:T(8,128)S(1)}, f32[8,32,128]{2,1,0:T(8,128)S(1)}, u32[]{:S(2)}, u32[]{:S(2)}) collective-permute-start(f32[8,32,128]{2,1,0:T(8,128)S(1)} %get-tuple-element.78), channel_id=1, source_target_pairs={{4,8},{0,12},{8,4},{12,0},{5,9},{1,13},{9,5},{13,1},{6,10},{2,14},... | collective-permute-start | bytes 393224 | tf_op jit(solution)/shard_map/ppermute | solution.py:119
  19.7 10.3 %collective-permute-start.6 = (f32[64,64]{1,0:T(8,128)S(1)}, f32[64,64]{1,0:T(8,128)S(1)}, u32[]{:S(2)}, u32[]{:S(2)}) collective-permute-start(f32[64,64]{1,0:T(8,128)S(1)} %gram.1), channel_id=1, source_target_pairs={{0,4},{4,0},{8,12},{12,8},{1,5},{5,1},{9,13},{13,9},{2,6},{6,2},{1... | collective-permute-start | bytes 49160 | tf_op jit(solution)/shard_map/ppermute | solution.py:140
  24.1 17.4 %collective-permute-start.8 = (f32[8,32,128]{2,1,0:T(8,128)S(1)}, f32[8,32,128]{2,1,0:T(8,128)S(1)}, u32[]{:S(2)}, u32[]{:S(2)}) collective-permute-start(f32[8,32,128]{2,1,0:T(8,128)S(1)} %get-tuple-element.92), channel_id=1, source_target_pairs={{4,8},{0,12},{8,4},{12,0},{5,9},{1,13},{9,5},{13,1},{6,10},{2,14},... | collective-permute-start | bytes 393224 | tf_op jit(solution)/shard_map/ppermute | solution.py:119
  25.4 8.4 %collective-permute-start.9 = (f32[8,32,128]{2,1,0:T(8,128)S(1)}, f32[8,32,128]{2,1,0:T(8,128)S(1)}, u32[]{:S(2)}, u32[]{:S(2)}) collective-permute-start(f32[8,32,128]{2,1,0:T(8,128)S(1)} %get-tuple-element.93), channel_id=1, source_target_pairs={{0,4},{8,12},{4,0},{12,8},{1,5},{9,13},{5,1},{13,9},{2,6},{10,14},... | collective-permute-start | bytes 393224 | tf_op jit(solution)/shard_map/ppermute | solution.py:119
  29.9 8.5 %collective-permute-start.10 = (f32[64,64]{1,0:T(8,128)S(1)}, f32[64,64]{1,0:T(8,128)S(1)}, u32[]{:S(2)}, u32[]{:S(2)}) collective-permute-start(f32[64,64]{1,0:T(8,128)S(1)} %add.46), channel_id=1, source_target_pairs={{0,8},{4,12},{8,0},{12,4},{1,9},{5,13},{9,1},{13,5},{2,10},{6,14},... | collective-permute-start | bytes 49160 | tf_op jit(solution)/shard_map/ppermute | solution.py:149
  31.1 12.7 %collective-permute-start.7 = (f32[8,32,128]{2,1,0:T(8,128)S(1)}, f32[8,32,128]{2,1,0:T(8,128)S(1)}, u32[]{:S(2)}, u32[]{:S(2)}) collective-permute-start(f32[8,32,128]{2,1,0:T(8,128)S(1)} %get-tuple-element.91), channel_id=1, source_target_pairs={{0,8},{4,12},{8,0},{12,4},{1,9},{5,13},{9,1},{13,5},{2,10},{6,14},... | collective-permute-start | bytes 393224 | tf_op jit(solution)/shard_map/ppermute | solution.py:119
  35.3 8.4 %collective-permute-start.13 = (f32[16,32,128]{2,1,0:T(8,128)S(1)}, f32[16,32,128]{2,1,0:T(8,128)S(1)}, u32[]{:S(2)}, u32[]{:S(2)}) collective-permute-start(f32[16,32,128]{2,1,0:T(8,128)S(1)} %add.47), channel_id=1, source_target_pairs={{0,2},{1,3},{2,0},{3,1},{4,6},{5,7},{6,4},{7,5},{8,10},{9,11},{10,... | collective-permute-start | bytes 786440 | tf_op jit(solution)/shard_map/ppermute | solution.py:502
  43.7 1.7 %collective-permute-start.14 = (f32[16,32,128]{2,1,0:T(8,128)S(1)}, f32[16,32,128]{2,1,0:T(8,128)S(1)}, u32[]{:S(2)}, u32[]{:S(2)}) collective-permute-start(f32[16,32,128]{2,1,0:T(8,128)S(1)} %add.49.refs_3_), channel_id=1, source_target_pairs={{0,1},{1,0},{2,3},{3,2},{4,5},{5,4},{6,7},{7,6},{8,9},{9,8},{10,11... | collective-permute-start | bytes 786440 | tf_op jit(solution)/shard_map/ppermute | solution.py:563
  44.9 2.1 %collective-permute-start.12 = (f32[16,32,128]{2,1,0:T(8,128)S(1)}, f32[16,32,128]{2,1,0:T(8,128)S(1)}, u32[]{:S(2)}, u32[]{:S(2)}) collective-permute-start(f32[16,32,128]{2,1,0:T(8,128)S(1)} %get-tuple-element.100), channel_id=1, source_target_pairs={{0,1},{1,0},{2,3},{3,2},{4,5},{5,4},{6,7},{7,6},{8,9},{9,8},{10,11... | collective-permute-start | bytes 786440 | tf_op jit(solution)/shard_map/ppermute | solution.py:567
  46.9 11.1 %collective-permute-start.17 = (f32[8,32,128]{2,1,0:T(8,128)S(1)}, f32[8,32,128]{2,1,0:T(8,128)S(1)}, u32[]{:S(2)}, u32[]{:S(2)}) collective-permute-start(f32[8,32,128]{2,1,0:T(8,128)S(1)} %get-tuple-element.106), channel_id=1, source_target_pairs={{0,8},{4,12},{8,0},{12,4},{1,9},{5,13},{9,1},{13,5},{2,10},{6,14},... | collective-permute-start | bytes 393224 | tf_op jit(solution)/shard_map/ppermute | solution.py:119
  47.0 12.9 %collective-permute-start.15 = (f32[16,32,128]{2,1,0:T(8,128)S(1)}, f32[16,32,128]{2,1,0:T(8,128)S(1)}, u32[]{:S(2)}, u32[]{:S(2)}) collective-permute-start(f32[16,32,128]{2,1,0:T(8,128)S(1)} %add.50), channel_id=1, source_target_pairs={{0,2},{1,3},{2,0},{3,1},{4,6},{5,7},{6,4},{7,5},{8,10},{9,11},{10,... | collective-permute-start | bytes 786440 | tf_op jit(solution)/shard_map/ppermute | solution.py:502
  50.3 8.6 %collective-permute-start.16 = (f32[8,32,128]{2,1,0:T(8,128)S(1)}, f32[8,32,128]{2,1,0:T(8,128)S(1)}, u32[]{:S(2)}, u32[]{:S(2)}) collective-permute-start(f32[8,32,128]{2,1,0:T(8,128)S(1)} %get-tuple-element.105), channel_id=1, source_target_pairs={{4,8},{0,12},{8,4},{12,0},{5,9},{1,13},{9,5},{13,1},{6,10},{2,14},... | collective-permute-start | bytes 393224 | tf_op jit(solution)/shard_map/ppermute | solution.py:119
  52.5 8.5 %collective-permute-start.19 = (f32[8,32,128]{2,1,0:T(8,128)S(1)}, f32[8,32,128]{2,1,0:T(8,128)S(1)}, u32[]{:S(2)}, u32[]{:S(2)}) collective-permute-start(f32[8,32,128]{2,1,0:T(8,128)S(1)} %get-tuple-element.110), channel_id=1, source_target_pairs={{0,4},{8,12},{4,0},{12,8},{1,5},{9,13},{5,1},{13,9},{2,6},{10,14},... | collective-permute-start | bytes 393224 | tf_op jit(solution)/shard_map/ppermute | solution.py:119
  59.9 2.1 %collective-permute-start.18 = (f32[16,32,128]{2,1,0:T(8,128)S(1)}, f32[16,32,128]{2,1,0:T(8,128)S(1)}, u32[]{:S(2)}, u32[]{:S(2)}) collective-permute-start(f32[16,32,128]{2,1,0:T(8,128)S(1)} %add.51.refs_3_), channel_id=1, source_target_pairs={{0,1},{1,0},{2,3},{3,2},{4,5},{5,4},{6,7},{7,6},{8,9},{9,8},{10,11... | collective-permute-start | bytes 786440 | tf_op jit(solution)/shard_map/ppermute | solution.py:573
  61.9 3.0 %collective-permute-start.23 = (f32[16,32,128]{2,1,0:T(8,128)S(1)}, f32[16,32,128]{2,1,0:T(8,128)S(1)}, u32[]{:S(2)}, u32[]{:S(2)}) collective-permute-start(f32[16,32,128]{2,1,0:T(8,128)S(1)} %get-tuple-element.119), channel_id=1, source_target_pairs={{0,1},{1,0},{2,3},{3,2},{4,5},{5,4},{6,7},{7,6},{8,9},{9,8},{10,11... | collective-permute-start | bytes 786440 | tf_op jit(solution)/shard_map/ppermute | solution.py:577
  63.7 10.8 %collective-permute-start.22 = (f32[8,32,128]{2,1,0:T(8,128)S(1)}, f32[8,32,128]{2,1,0:T(8,128)S(1)}, u32[]{:S(2)}, u32[]{:S(2)}) collective-permute-start(f32[8,32,128]{2,1,0:T(8,128)S(1)} %get-tuple-element.115), channel_id=1, source_target_pairs={{0,8},{4,12},{8,0},{12,4},{1,9},{5,13},{9,1},{13,5},{2,10},{6,14},... | collective-permute-start | bytes 393224 | tf_op jit(solution)/shard_map/ppermute | solution.py:119
  66.1 8.4 %collective-permute-start.24 = (f32[64,128]{1,0:T(8,128)S(1)}, f32[64,128]{1,0:T(8,128)S(1)}, u32[]{:S(2)}, u32[]{:S(2)}) collective-permute-start(f32[64,128]{1,0:T(8,128)S(1)} %cross.1), channel_id=1, source_target_pairs={{0,4},{4,0},{8,12},{12,8},{1,5},{5,1},{9,13},{13,9},{2,6},{6,2},{1... | collective-permute-start | bytes 98312 | tf_op jit(solution)/shard_map/ppermute | solution.py:140
  66.8 15.6 %collective-permute-start.28 = (f32[16,32,128]{2,1,0:T(8,128)S(1)}, f32[16,32,128]{2,1,0:T(8,128)S(1)}, u32[]{:S(2)}, u32[]{:S(2)}) collective-permute-start(f32[16,32,128]{2,1,0:T(8,128)S(1)} %add.52), channel_id=1, source_target_pairs={{0,2},{1,3},{2,0},{3,1},{4,6},{5,7},{6,4},{7,5},{8,10},{9,11},{10,... | collective-permute-start | bytes 786440 | tf_op jit(solution)/shard_map/ppermute | solution.py:502
  70.0 11.3 %collective-permute-start.20 = (f32[8,32,128]{2,1,0:T(8,128)S(1)}, f32[8,32,128]{2,1,0:T(8,128)S(1)}, u32[]{:S(2)}, u32[]{:S(2)}) collective-permute-start(f32[8,32,128]{2,1,0:T(8,128)S(1)} %get-tuple-element.113), channel_id=1, source_target_pairs={{0,4},{8,12},{4,0},{12,8},{1,5},{9,13},{5,1},{13,9},{2,6},{10,14},... | collective-permute-start | bytes 393224 | tf_op jit(solution)/shard_map/ppermute | solution.py:119
  71.5 8.8 %collective-permute-start.21 = (f32[8,32,128]{2,1,0:T(8,128)S(1)}, f32[8,32,128]{2,1,0:T(8,128)S(1)}, u32[]{:S(2)}, u32[]{:S(2)}) collective-permute-start(f32[8,32,128]{2,1,0:T(8,128)S(1)} %get-tuple-element.114), channel_id=1, source_target_pairs={{4,8},{0,12},{8,4},{12,0},{5,9},{1,13},{9,5},{13,1},{6,10},{2,14},... | collective-permute-start | bytes 393224 | tf_op jit(solution)/shard_map/ppermute | solution.py:119
  74.4 6.8 %collective-permute-start.25 = (f32[64,128]{1,0:T(8,128)S(1)}, f32[64,128]{1,0:T(8,128)S(1)}, u32[]{:S(2)}, u32[]{:S(2)}) collective-permute-start(f32[64,128]{1,0:T(8,128)S(1)} %add.53), channel_id=1, source_target_pairs={{0,8},{4,12},{8,0},{12,4},{1,9},{5,13},{9,1},{13,5},{2,10},{6,14},... | collective-permute-start | bytes 98312 | tf_op jit(solution)/shard_map/ppermute | solution.py:149
  82.3 1.6 %collective-permute-start.26 = (f32[16,32,128]{2,1,0:T(8,128)S(1)}, f32[16,32,128]{2,1,0:T(8,128)S(1)}, u32[]{:S(2)}, u32[]{:S(2)}) collective-permute-start(f32[16,32,128]{2,1,0:T(8,128)S(1)} %get-tuple-element.127), channel_id=1, source_target_pairs={{0,1},{1,0},{2,3},{3,2},{4,5},{5,4},{6,7},{7,6},{8,9},{9,8},{10,11... | collective-permute-start | bytes 786440 | tf_op jit(solution)/shard_map/ppermute | solution.py:590
  82.4 6.2 %collective-permute-start.29 = (f32[16,32,128]{2,1,0:T(8,128)S(1)}, f32[16,32,128]{2,1,0:T(8,128)S(1)}, u32[]{:S(2)}, u32[]{:S(2)}) collective-permute-start(f32[16,32,128]{2,1,0:T(8,128)S(1)} %add.56.mine_ref), channel_id=1, source_target_pairs={{0,1},{1,0},{2,3},{3,2},{4,5},{5,4},{6,7},{7,6},{8,9},{9,8},{10,11... | collective-permute-start | bytes 786440 | tf_op jit(solution)/shard_map/ppermute | solution.py:587
  83.9 8.4 %collective-permute-start.27 = (f32[16,32,128]{2,1,0:T(8,128)S(1)}, f32[16,32,128]{2,1,0:T(8,128)S(1)}, u32[]{:S(2)}, u32[]{:S(2)}) collective-permute-start(f32[16,32,128]{2,1,0:T(8,128)S(1)} %add.55), channel_id=1, source_target_pairs={{0,2},{1,3},{2,0},{3,1},{4,6},{5,7},{6,4},{7,5},{8,10},{9,11},{10,... | collective-permute-start | bytes 786440 | tf_op jit(solution)/shard_map/ppermute | solution.py:502
  92.4 1.6 %collective-permute-start.30 = (f32[16,32,128]{2,1,0:T(8,128)S(1)}, f32[16,32,128]{2,1,0:T(8,128)S(1)}, u32[]{:S(2)}, u32[]{:S(2)}) collective-permute-start(f32[16,32,128]{2,1,0:T(8,128)S(1)} %add.57.mine_ref), channel_id=1, source_target_pairs={{0,1},{1,0},{2,3},{3,2},{4,5},{5,4},{6,7},{7,6},{8,9},{9,8},{10,11... | collective-permute-start | bytes 786440 | tf_op jit(solution)/shard_map/ppermute | solution.py:598
  96.0 4.0 %collective-permute-start.31 = (f32[72,128]{1,0:T(8,128)S(1)}, f32[72,128]{1,0:T(8,128)S(1)}, u32[]{:S(2)}, u32[]{:S(2)}) collective-permute-start(f32[72,128]{1,0:T(8,128)S(1)} %get-tuple-element.140), channel_id=1, source_target_pairs={{0,4},{4,0},{8,12},{12,8},{1,5},{5,1},{9,13},{13,9},{2,6},{6,2},{1... | collective-permute-start | bytes 110600 | tf_op jit(solution)/shard_map/ppermute | solution.py:140
  100.0 5.3 %collective-permute-start.32 = (f32[72,128]{1,0:T(8,128)S(1)}, f32[72,128]{1,0:T(8,128)S(1)}, u32[]{:S(2)}, u32[]{:S(2)}) collective-permute-start(f32[72,128]{1,0:T(8,128)S(1)} %add.58), channel_id=1, source_target_pairs={{0,8},{4,12},{8,0},{12,4},{1,9},{5,13},{9,1},{13,5},{2,10},{6,14},... | collective-permute-start | bytes 110600 | tf_op jit(solution)/shard_map/ppermute | solution.py:149
  (5 other events, 29.2 us)

commit v9 on v8

--- a/solution.py
+++ b/solution.py
@@ -542,15 +542,16 @@
     acc_a, acc_b = own(x, after(acc_a, sent[0]), acc_b)
     for n in range(2):
         acc_a = join(acc_a, got_a, groups[n])
-        acc_a, x, *gated = lax.optimization_barrier((acc_a, x, *[sent_b[p] for p in groups[n]]))
-        for p, value in zip(groups[n], gated):
+        turn = groups[0] if n == 1 else []
+        acc_a, x, *gated = lax.optimization_barrier((acc_a, x, *[sent_b[p] for p in turn]))
+        for p, value in zip(turn, gated):
             sent_b[p] = value
         if n == 0:
             (gram,) = call(gram_body, [square], [VMEM], name="gram")(x)
             start_gram = start_sum(gram, "res")
     acc_a = after(acc_a, start_gram)
     keep_a, give_a = join(acc_a, got_a, groups[2], last=True)
-    for p in groups[2]:
+    for p in groups[1] + groups[2]:
         sent_b[p] = after(sent_b[p], keep_a)
     got_b = spread(sent_b)
 
@@ -577,9 +578,9 @@
     core = lax.ppermute(give_a, "vec", swap)
     mine_a = keep_a + after(core, y_b)
     (gram,) = call(cross_body, [(width, 2 * width)], [VMEM] * 3, name="cross")(x, y_a, after(y_b, mine_a))
-    (acc_b,) = own(y_b, after(acc_b, gram))
     cross_gram = start_sum(gram, "res")
     acc_b = join(after(acc_b, cross_gram), got_b, groups[2])
+    (acc_b,) = own(y_b, acc_b)
     acc_b = join(acc_b, got_b, groups[1])
     cross_gram = end_sum(cross_gram, "res", acc_b)
     acc_b = after(acc_b, cross_gram)

time: 111 us -> 111 us (level)
    ppermute x3, waiting for transfers between devices: 5.53 us -> 7.25 us  [end_sum(): got = lax.ppermute(block, axis, [(i, i ^ step) for i in range(size)])]
    ppermute x15, waiting for transfers between devices: 13.6 us -> 12.1 us  [exchange(): lax.ppermute(block, axis, [(a, b) for a, b in pairs] + [(b, a) for a, b i...]
    ppermute x15, starting transfers between devices: 28 us -> 26.5 us  [exchange(): lax.ppermute(block, axis, [(a, b) for a, b in pairs] + [(b, a) for a, b i...]
  transfers between devices with their start and end apart: 33 -> 33, of which waited for: 14 -> 13; matrix products, arithmetic and copies ran while one was open for 1% -> 1% of each run, Pallas kernels for 31% -> 31%
where the time goes in v9:
time: 111 us
  Pallas kernels  43.4 us (39%)
  starting transfers between devices  38.8 us (35%)
  waiting for transfers between devices  26.3 us (24%)
    ppermute x15, starting transfers between devices, exchange(): lax.ppermute(block, axis, [(a, b) for a, b in pairs] + [(b, a) for a, b i...  26.5 us
    ppermute x15, waiting for transfers between devices, exchange(): lax.ppermute(block, axis, [(a, b) for a, b in pairs] + [(b, a) for a, b i...  12.1 us
    pallas_call x12, Pallas kernels, join(): call(body, [halfchunk] * 2 if last else [chunk], [SMEM] * (3 + size) + [V...  11.7 us
    ppermute x3, waiting for transfers between devices, end_sum(): got = lax.ppermute(block, axis, [(i, i ^ step) for i in range(size)])  7.25 us
    ppermute x4, starting transfers between devices, across(): got = lax.ppermute(mine, 'vec', [(i, i ^ step) for i in range(lanes)])  6.14 us
    pallas_call x3, Pallas kernels, own(): call(own_body, [chunk] * len(accs), [SMEM] * 2 + [VMEM] * (2 + len(accs))...  5.46 us
    pallas_call x1, Pallas kernels, local(): call(second_body, [square, square, (2 * width, 3 * width), square], [VMEM...  3.94 us
    pallas_call x1, Pallas kernels, local(): call(fourth_body, [square, square, (width, 2 * width)], [VMEM], name='fou...  3.7 us
  transfers between devices with their start and end apart: 33, of which 13 were waited for; matrix products, arithmetic and copies ran while one was open for 1% of the time, Pallas kernels for 31%

profile of v9, /device:TPU:0, one launch (start us, length us, event | category | flops | bytes accessed | tf_op | source)
XLA Modules:
  0.0 110.7 jit_solution(12778730244322096680)
XLA Ops:
  0.6 4.1 %collective-permute-start.2 = (s32[1,1,44]{2,1,0:T(1,128)}, s32[1,1,44]{2,1,0:T(1,128)S(1)}, u32[]{:S(2)}, u32[]{:S(2)}) collective-permute-start(s32[1,1,44]{2,1,0:T(1,128)} %cols_ref.5), channel_id=1, source_target_pairs={{0,8},{4,12},{8,0},{12,4},{1,9},{5,13},{9,1},{13,5},{2,10},{6,14},... | collective-permute-start | bytes 536 | tf_op jit(solution)/shard_map/ppermute | solution.py:119
  7.1 2.3 %prepare.1 = (f32[32,64,128]{2,1,0:T(8,128)S(1)}, bf16[44,2,128,128]{3,2,1,0:T(8,128)(2,1)S(1)}, f32[32,32,128]{2,1,0:T(8,128)S(1)}, f32[32,32,128]{2,1,0:T(8,128)S(1)}) custom-call(f32[32,64,128]{2,1,0:T(8,128)} %x_hbm.1, f32[32,128]{1,0:T(8,128)} %refs_5_.3, f32[1,1,44,128,128]{4,3,2,1,0:T(8,128)} %tiles_hbm.1), custom_call_target="tpu_custom_call" | custom-call | tf_op jit(solution)/shard_map/prepare/pallas_call | solution.py:526
  10.2 1.4 %send.1 = (f32[8,32,128]{2,1,0:T(8,128)S(1)}, f32[8,32,128]{2,1,0:T(8,128)S(1)}, f32[8,32,128]{2,1,0:T(8,128)S(1)}, f32[8,32,128]{2,1,0:T(8,128)S(1)}, f32[8,32,...) custom-call(s32[4]{0:T(128)S(1)} %pad_add_fusion.place_ref, s32[1,1,44]{2,1,0:T(1,128)S(1)} %copy-done.1, ...), custom_call_target="tpu_custom_call" | custom-call | tf_op jit(solution)/shard_map/send/pallas_call | solution.py:537
  13.7 2.4 %collective-permute-start.4 = (f32[8,32,128]{2,1,0:T(8,128)S(1)}, f32[8,32,128]{2,1,0:T(8,128)S(1)}, u32[]{:S(2)}, u32[]{:S(2)}) collective-permute-start(f32[8,32,128]{2,1,0:T(8,128)S(1)} %get-tuple-element.77), channel_id=1, source_target_pairs={{4,8},{0,12},{8,4},{12,0},{5,9},{1,13},{9,5},{13,1},{6,10},{2,14},... | collective-permute-start | bytes 393224 | tf_op jit(solution)/shard_map/ppermute | solution.py:119
  16.1 2.0 %own.3 = (f32[32,32,128]{2,1,0:T(8,128)S(1)}, f32[32,32,128]{2,1,0:T(8,128)S(1)}) custom-call(s32[1,1,44]{2,1,0:T(1,128)S(1)} %copy-done.1, s32[1,1,44]{2,1,0:T(1,128)S(1)} %copy-done.2, f32[32,64,128]{2,1,0:T(8,128)S(1)} %get-tuple-element.117.refs_3_.x_ref, ...), custom_call_target="tpu_custom_call", output_to_operand_aliasing={{0}: (4, {}), {1}: (5, {})} | custom-call | tf_op jit(solution)/shard_map/own/pallas_call | solution.py:517
  20.2 2.9 %collective-permute-done.4.refs_1_ = f32[8,32,128]{2,1,0:T(8,128)S(1)} collective-permute-done((f32[8,32,128]{2,1,0:T(8,128)S(1)}, f32[8,32,128]{2,1,0:T(8,128)S(1)}, u32[]{:S(2)}, u32[]{:S(2)}) %collective-permute-start.4) | collective-permute-done | bytes 131104 | tf_op jit(solution)/shard_map/ppermute | solution.py:119
  24.1 3.5 %collective-permute-start.9 = (f32[8,32,128]{2,1,0:T(8,128)S(1)}, f32[8,32,128]{2,1,0:T(8,128)S(1)}, u32[]{:S(2)}, u32[]{:S(2)}) collective-permute-start(f32[8,32,128]{2,1,0:T(8,128)S(1)} %get-tuple-element.92), channel_id=1, source_target_pairs={{0,4},{8,12},{4,0},{12,8},{1,5},{9,13},{5,1},{13,9},{2,6},{10,14},... | collective-permute-start | bytes 393224 | tf_op jit(solution)/shard_map/ppermute | solution.py:119
  29.1 2.2 %collective-permute-start.7 = (f32[8,32,128]{2,1,0:T(8,128)S(1)}, f32[8,32,128]{2,1,0:T(8,128)S(1)}, u32[]{:S(2)}, u32[]{:S(2)}) collective-permute-start(f32[8,32,128]{2,1,0:T(8,128)S(1)} %get-tuple-element.89), channel_id=1, source_target_pairs={{0,8},{4,12},{8,0},{12,4},{1,9},{5,13},{9,1},{13,5},{2,10},{6,14},... | collective-permute-start | bytes 393224 | tf_op jit(solution)/shard_map/ppermute | solution.py:119
  31.3 2.2 %collective-permute-start.8 = (f32[8,32,128]{2,1,0:T(8,128)S(1)}, f32[8,32,128]{2,1,0:T(8,128)S(1)}, u32[]{:S(2)}, u32[]{:S(2)}) collective-permute-start(f32[8,32,128]{2,1,0:T(8,128)S(1)} %get-tuple-element.91), channel_id=1, source_target_pairs={{4,8},{0,12},{8,4},{12,0},{5,9},{1,13},{9,5},{13,1},{6,10},{2,14},... | collective-permute-start | bytes 393224 | tf_op jit(solution)/shard_map/ppermute | solution.py:119
  35.1 1.6 %collective-permute-start.13 = (f32[16,32,128]{2,1,0:T(8,128)S(1)}, f32[16,32,128]{2,1,0:T(8,128)S(1)}, u32[]{:S(2)}, u32[]{:S(2)}) collective-permute-start(f32[16,32,128]{2,1,0:T(8,128)S(1)} %add.47), channel_id=1, source_target_pairs={{0,2},{1,3},{2,0},{3,1},{4,6},{5,7},{6,4},{7,5},{8,10},{9,11},{10,... | collective-permute-start | bytes 786440 | tf_op jit(solution)/shard_map/ppermute | solution.py:502
  36.7 2.1 %collective-permute-done.10 = f32[64,64]{1,0:T(8,128)S(1)} collective-permute-done((f32[64,64]{1,0:T(8,128)S(1)}, f32[64,64]{1,0:T(8,128)S(1)}, u32[]{:S(2)}, u32[]{:S(2)}) %collective-permute-start.10) | collective-permute-done | bytes 16416 | tf_op jit(solution)/shard_map/ppermute | solution.py:149
  38.8 3.0 %first.1.inverse_ref = f32[64,64]{1,0:T(8,128)S(1)} custom-call(f32[64,64]{1,0:T(8,128)S(1)} %add.48.gram_ref), custom_call_target="tpu_custom_call" | custom-call | tf_op jit(solution)/shard_map/first/pallas_call | solution.py:561
  45.3 1.4 %resend.2 = (f32[32,32,128]{2,1,0:T(8,128)S(1)}, f32[32,32,128]{2,1,0:T(8,128)S(1)}, f32[8,32,128]{2,1,0:T(8,128)S(1)}, f32[8,32,128]{2,1,0:T(8,128)S(1)}, f32[8,32,128]{2,1,0:T(8,128)S(1)}) custom-call(s32[4]{0:T(128)S(1)} %pad_add_fusion.place_ref, s32[1,1,44]{2,1,0:T(1,128)S(1)} %copy-done.1, s32[1,1,3]{2,1,0:T(1,128)S(1)} %copy-done.3, ...), custom_call_target="tpu_custom_call" | custom-call | tf_op jit(solution)/shard_map/resend/pallas_call | solution.py:508
  47.3 1.5 %collective-permute-start.15 = (f32[16,32,128]{2,1,0:T(8,128)S(1)}, f32[16,32,128]{2,1,0:T(8,128)S(1)}, u32[]{:S(2)}, u32[]{:S(2)}) collective-permute-start(f32[16,32,128]{2,1,0:T(8,128)S(1)} %add.50), channel_id=1, source_target_pairs={{0,2},{1,3},{2,0},{3,1},{4,6},{5,7},{6,4},{7,5},{8,10},{9,11},{10,... | collective-permute-start | bytes 786440 | tf_op jit(solution)/shard_map/ppermute | solution.py:502
  48.8 1.7 %own.4.refs_3_ = f32[32,32,128]{2,1,0:T(8,128)S(1)} custom-call(s32[1,1,44]{2,1,0:T(1,128)S(1)} %copy-done.1, s32[1,1,44]{2,1,0:T(1,128)S(1)} %copy-done.2, f32[32,32,128]{2,1,0:T(8,128)S(1)} %get-tuple-element.102.x_ref.a_ref, bf16[44,2,128,128]{3,2,1,0:T(8,128)(2,1)S(1)} %get-tuple-element.74.refs_4_.split_ref.refs_2_.refs_6_, ...), custom_call_target="tpu_custom_call", output_to_operand_aliasing={{}: (4, {})} | custom-call | tf_op jit(solution)/shard_map/own/pallas_call | solution.py:517
  50.5 3.1 %collective-permute-start.16 = (f32[8,32,128]{2,1,0:T(8,128)S(1)}, f32[8,32,128]{2,1,0:T(8,128)S(1)}, u32[]{:S(2)}, u32[]{:S(2)}) collective-permute-start(f32[8,32,128]{2,1,0:T(8,128)S(1)} %get-tuple-element.104), channel_id=1, source_target_pairs={{4,8},{0,12},{8,4},{12,0},{5,9},{1,13},{9,5},{13,1},{6,10},{2,14},... | collective-permute-start | bytes 393224 | tf_op jit(solution)/shard_map/ppermute | solution.py:119
  53.7 5.8 %collective-permute-done.17.refs_1_ = f32[8,32,128]{2,1,0:T(8,128)S(1)} collective-permute-done((f32[8,32,128]{2,1,0:T(8,128)S(1)}, f32[8,32,128]{2,1,0:T(8,128)S(1)}, u32[]{:S(2)}, u32[]{:S(2)}) %collective-permute-start.17) | collective-permute-done | bytes 131104 | tf_op jit(solution)/shard_map/ppermute | solution.py:119
  63.1 1.6 %resend.3 = (f32[32,32,128]{2,1,0:T(8,128)S(1)}, f32[32,32,128]{2,1,0:T(8,128)S(1)}, f32[8,32,128]{2,1,0:T(8,128)S(1)}, f32[8,32,128]{2,1,0:T(8,128)S(1)}, f32[8,32,128]{2,1,0:T(8,128)S(1)}) custom-call(s32[4]{0:T(128)S(1)} %pad_add_fusion.place_ref, s32[1,1,44]{2,1,0:T(1,128)S(1)} %copy-done.1, s32[1,1,3]{2,1,0:T(1,128)S(1)} %copy-done.3, ...), custom_call_target="tpu_custom_call" | custom-call | tf_op jit(solution)/shard_map/resend/pallas_call | solution.py:508
  67.4 1.5 %collective-permute-start.28 = (f32[16,32,128]{2,1,0:T(8,128)S(1)}, f32[16,32,128]{2,1,0:T(8,128)S(1)}, u32[]{:S(2)}, u32[]{:S(2)}) collective-permute-start(f32[16,32,128]{2,1,0:T(8,128)S(1)} %add.52), channel_id=1, source_target_pairs={{0,2},{1,3},{2,0},{3,1},{4,6},{5,7},{6,4},{7,5},{8,10},{9,11},{10,... | collective-permute-start | bytes 786440 | tf_op jit(solution)/shard_map/ppermute | solution.py:502
  69.8 3.5 %collective-permute-start.21 = (f32[8,32,128]{2,1,0:T(8,128)S(1)}, f32[8,32,128]{2,1,0:T(8,128)S(1)}, u32[]{:S(2)}, u32[]{:S(2)}) collective-permute-start(f32[8,32,128]{2,1,0:T(8,128)S(1)} %get-tuple-element.113), channel_id=1, source_target_pairs={{4,8},{0,12},{8,4},{12,0},{5,9},{1,13},{9,5},{13,1},{6,10},{2,14},... | collective-permute-start | bytes 393224 | tf_op jit(solution)/shard_map/ppermute | solution.py:119
  73.8 1.8 %collective-permute-done.22.refs_1_ = f32[8,32,128]{2,1,0:T(8,128)S(1)} collective-permute-done((f32[8,32,128]{2,1,0:T(8,128)S(1)}, f32[8,32,128]{2,1,0:T(8,128)S(1)}, u32[]{:S(2)}, u32[]{:S(2)}) %collective-permute-start.22) | collective-permute-done | bytes 131104 | tf_op jit(solution)/shard_map/ppermute | solution.py:119
  76.5 1.7 %own.5.refs_3_ = f32[32,32,128]{2,1,0:T(8,128)S(1)} custom-call(s32[1,1,44]{2,1,0:T(1,128)S(1)} %copy-done.1, s32[1,1,44]{2,1,0:T(1,128)S(1)} %copy-done.2, f32[32,32,128]{2,1,0:T(8,128)S(1)} %get-tuple-element.120.b_ref.x_ref, bf16[44,2,128,128]{3,2,1,0:T(8,128)(2,1)S(1)} %get-tuple-element.74.refs_4_.split_ref.refs_2_.refs_6_, ...), custom_call_target="tpu_custom_call", output_to_operand_aliasing={{}: (4, {})} | custom-call | tf_op jit(solution)/shard_map/own/pallas_call | solution.py:517
  83.7 1.5 %collective-permute-start.27 = (f32[16,32,128]{2,1,0:T(8,128)S(1)}, f32[16,32,128]{2,1,0:T(8,128)S(1)}, u32[]{:S(2)}, u32[]{:S(2)}) collective-permute-start(f32[16,32,128]{2,1,0:T(8,128)S(1)} %add.55), channel_id=1, source_target_pairs={{0,2},{1,3},{2,0},{3,1},{4,6},{5,7},{6,4},{7,5},{8,10},{9,11},{10,... | collective-permute-start | bytes 786440 | tf_op jit(solution)/shard_map/ppermute | solution.py:502
  85.2 3.9 %second.1 = (f32[64,64]{1,0:T(8,128)S(1)}, f32[64,64]{1,0:T(8,128)S(1)}, f32[128,192]{1,0:T(8,128)S(1)}, f32[64,64]{1,0:T(8,128)S(1)}) custom-call(f32[64,128]{1,0:T(8,128)S(1)} %add.54.gram_ref, f32[64,64]{1,0:T(8,128)S(1)} %first.1.inverse_ref), custom_call_target="tpu_custom_call" | custom-call | tf_op jit(solution)/shard_map/second/pallas_call | solution.py:593
  89.2 1.7 %blend.3 = (f32[16,64,128]{2,1,0:T(8,128)S(1)}, f32[16,64,128]{2,1,0:T(8,128)S(1)}, f32[64,64]{1,0:T(8,128)S(1)}) custom-call(s32[4]{0:T(128)S(1)} %pad_add_fusion.place_ref, f32[32,64,128]{2,1,0:T(8,128)S(1)} %get-tuple-element.117.refs_3_.x_ref, f32[32,32,128]{2,1,0:T(8,128)S(1)} %get-tuple-element.102.x_ref.a_ref, ...), custom_call_target="tpu_custom_call" | custom-call | tf_op jit(solution)/shard_map/blend/pallas_call | solution.py:436
  90.9 1.7 %blend.2 = (f32[16,64,128]{2,1,0:T(8,128)S(1)}, f32[16,64,128]{2,1,0:T(8,128)S(1)}, f32[64,64]{1,0:T(8,128)S(1)}) custom-call(s32[4]{0:T(128)S(1)} %pad_add_fusion.place_ref, f32[32,64,128]{2,1,0:T(8,128)S(1)} %get-tuple-element.117.refs_3_.x_ref, f32[32,32,128]{2,1,0:T(8,128)S(1)} %get-tuple-element.102.x_ref.a_ref, ...), custom_call_target="tpu_custom_call" | custom-call | tf_op jit(solution)/shard_map/blend/pallas_call | solution.py:436
  92.8 1.5 %collective-permute-done.30.other_ref = f32[16,32,128]{2,1,0:T(8,128)S(1)} collective-permute-done((f32[16,32,128]{2,1,0:T(8,128)S(1)}, f32[16,32,128]{2,1,0:T(8,128)S(1)}, u32[]{:S(2)}, u32[]{:S(2)}) %collective-permute-start.30) | collective-permute-done | bytes 262176 | tf_op jit(solution)/shard_map/ppermute | solution.py:599
  94.3 2.0 %third.1 = (f32[32,64,128]{2,1,0:T(8,128)S(1)}, f32[72,128]{1,0:T(8,128)S(1)}) custom-call(s32[4]{0:T(128)S(1)} %pad_add_fusion.place_ref, f32[16,32,128]{2,1,0:T(8,128)S(1)} %add.57.mine_ref, f32[16,32,128]{2,1,0:T(8,128)S(1)} %collective-permute-done.30.other_ref, f32[64,64]{1,0:T(8,128)S(1)} %get-tuple-element.132.gain_ref, ...), custom_call_target="tpu_custom_call" | custom-call | tf_op jit(solution)/shard_map/third/pallas_call | solution.py:600
  97.2 3.1 %collective-permute-done.31 = f32[72,128]{1,0:T(8,128)S(1)} collective-permute-done((f32[72,128]{1,0:T(8,128)S(1)}, f32[72,128]{1,0:T(8,128)S(1)}, u32[]{:S(2)}, u32[]{:S(2)}) %collective-permute-start.31) | collective-permute-done | bytes 36896 | tf_op jit(solution)/shard_map/ppermute | solution.py:140
  101.0 4.2 %collective-permute-done.32 = f32[72,128]{1,0:T(8,128)S(1)} collective-permute-done((f32[72,128]{1,0:T(8,128)S(1)}, f32[72,128]{1,0:T(8,128)S(1)}, u32[]{:S(2)}, u32[]{:S(2)}) %collective-permute-start.32) | collective-permute-done | bytes 36896 | tf_op jit(solution)/shard_map/ppermute | solution.py:149
  105.2 3.7 %fourth.1 = (f32[64,64]{1,0:T(8,128)S(1)}, f32[64,64]{1,0:T(8,128)S(1)}, f32[64,128]{1,0:T(8,128)S(1)}) custom-call(f32[72,128]{1,0:T(8,128)S(1)} %add.59.gram_ref), custom_call_target="tpu_custom_call" | custom-call | tf_op jit(solution)/shard_map/fourth/pallas_call | solution.py:608
  108.9 1.9 %last.1 = (f32[32,64,128]{2,1,0:T(8,128)}, f32[4,64,64]{2,1,0:T(8,128)}) custom-call(f32[32,64,128]{2,1,0:T(8,128)S(1)} %get-tuple-element.137.w_ref, f32[16,64,128]{2,1,0:T(8,128)S(1)} %get-tuple-element.135.refs_2_.low_ref, f32[16,64,128]{2,1,0:T(8,128)S(1)} %get-tuple-element.136.refs_3_.high_ref, f32[64,128]{1,0:T(8,128)S(1)} %get-tuple-element.139.coef_ref, ...), custom_call_target="tpu_custom_call" | custom-call | tf_op jit(solution)/shard_map/last/pallas_call | solution.py:611
  (86 shorter events, 30.9 us)
Async XLA Ops:
  0.6 8.8 %collective-permute-start.2 = (s32[1,1,44]{2,1,0:T(1,128)}, s32[1,1,44]{2,1,0:T(1,128)S(1)}, u32[]{:S(2)}, u32[]{:S(2)}) collective-permute-start(s32[1,1,44]{2,1,0:T(1,128)} %cols_ref.5), channel_id=1, source_target_pairs={{0,8},{4,12},{8,0},{12,4},{1,9},{5,13},{9,1},{13,5},{2,10},{6,14},... | collective-permute-start | bytes 536 | tf_op jit(solution)/shard_map/ppermute | solution.py:119
  4.8 5.5 %collective-permute-start.1 = (s32[1,1,44]{2,1,0:T(1,128)}, s32[1,1,44]{2,1,0:T(1,128)S(1)}, u32[]{:S(2)}, u32[]{:S(2)}) collective-permute-start(s32[1,1,44]{2,1,0:T(1,128)} %cols_ref.5), channel_id=1, source_target_pairs={{4,8},{0,12},{8,4},{12,0},{5,9},{1,13},{9,5},{13,1},{6,10},{2,14},... | collective-permute-start | bytes 536 | tf_op jit(solution)/shard_map/ppermute | solution.py:119
  6.1 4.1 %collective-permute-start = (s32[1,1,44]{2,1,0:T(1,128)}, s32[1,1,44]{2,1,0:T(1,128)S(1)}, u32[]{:S(2)}, u32[]{:S(2)}) collective-permute-start(s32[1,1,44]{2,1,0:T(1,128)} %cols_ref.5), channel_id=1, source_target_pairs={{0,4},{8,12},{4,0},{12,8},{1,5},{9,13},{5,1},{13,9},{2,6},{10,14},... | collective-permute-start | bytes 536 | tf_op jit(solution)/shard_map/ppermute | solution.py:119
  11.7 6.5 %collective-permute-start.5 = (f32[8,32,128]{2,1,0:T(8,128)S(1)}, f32[8,32,128]{2,1,0:T(8,128)S(1)}, u32[]{:S(2)}, u32[]{:S(2)}) collective-permute-start(f32[8,32,128]{2,1,0:T(8,128)S(1)} %get-tuple-element.78), channel_id=1, source_target_pairs={{0,4},{8,12},{4,0},{12,8},{1,5},{9,13},{5,1},{13,9},{2,6},{10,14},... | collective-permute-start | bytes 393224 | tf_op jit(solution)/shard_map/ppermute | solution.py:119
  12.5 15.5 %collective-permute-start.3 = (f32[8,32,128]{2,1,0:T(8,128)S(1)}, f32[8,32,128]{2,1,0:T(8,128)S(1)}, u32[]{:S(2)}, u32[]{:S(2)}) collective-permute-start(f32[8,32,128]{2,1,0:T(8,128)S(1)} %get-tuple-element.76), channel_id=1, source_target_pairs={{0,8},{4,12},{8,0},{12,4},{1,9},{5,13},{9,1},{13,5},{2,10},{6,14},... | collective-permute-start | bytes 393224 | tf_op jit(solution)/shard_map/ppermute | solution.py:119
  13.7 9.4 %collective-permute-start.4 = (f32[8,32,128]{2,1,0:T(8,128)S(1)}, f32[8,32,128]{2,1,0:T(8,128)S(1)}, u32[]{:S(2)}, u32[]{:S(2)}) collective-permute-start(f32[8,32,128]{2,1,0:T(8,128)S(1)} %get-tuple-element.77), channel_id=1, source_target_pairs={{4,8},{0,12},{8,4},{12,0},{5,9},{1,13},{9,5},{13,1},{6,10},{2,14},... | collective-permute-start | bytes 393224 | tf_op jit(solution)/shard_map/ppermute | solution.py:119
  19.7 7.9 %collective-permute-start.6 = (f32[64,64]{1,0:T(8,128)S(1)}, f32[64,64]{1,0:T(8,128)S(1)}, u32[]{:S(2)}, u32[]{:S(2)}) collective-permute-start(f32[64,64]{1,0:T(8,128)S(1)} %gram.1), channel_id=1, source_target_pairs={{0,4},{4,0},{8,12},{12,8},{1,5},{5,1},{9,13},{13,9},{2,6},{6,2},{1... | collective-permute-start | bytes 49160 | tf_op jit(solution)/shard_map/ppermute | solution.py:140
  24.1 9.5 %collective-permute-start.9 = (f32[8,32,128]{2,1,0:T(8,128)S(1)}, f32[8,32,128]{2,1,0:T(8,128)S(1)}, u32[]{:S(2)}, u32[]{:S(2)}) collective-permute-start(f32[8,32,128]{2,1,0:T(8,128)S(1)} %get-tuple-element.92), channel_id=1, source_target_pairs={{0,4},{8,12},{4,0},{12,8},{1,5},{9,13},{5,1},{13,9},{2,6},{10,14},... | collective-permute-start | bytes 393224 | tf_op jit(solution)/shard_map/ppermute | solution.py:119
  27.6 11.2 %collective-permute-start.10 = (f32[64,64]{1,0:T(8,128)S(1)}, f32[64,64]{1,0:T(8,128)S(1)}, u32[]{:S(2)}, u32[]{:S(2)}) collective-permute-start(f32[64,64]{1,0:T(8,128)S(1)} %add.46), channel_id=1, source_target_pairs={{0,8},{4,12},{8,0},{12,4},{1,9},{5,13},{9,1},{13,5},{2,10},{6,14},... | collective-permute-start | bytes 49160 | tf_op jit(solution)/shard_map/ppermute | solution.py:149
  29.1 14.5 %collective-permute-start.7 = (f32[8,32,128]{2,1,0:T(8,128)S(1)}, f32[8,32,128]{2,1,0:T(8,128)S(1)}, u32[]{:S(2)}, u32[]{:S(2)}) collective-permute-start(f32[8,32,128]{2,1,0:T(8,128)S(1)} %get-tuple-element.89), channel_id=1, source_target_pairs={{0,8},{4,12},{8,0},{12,4},{1,9},{5,13},{9,1},{13,5},{2,10},{6,14},... | collective-permute-start | bytes 393224 | tf_op jit(solution)/shard_map/ppermute | solution.py:119
  31.3 10.4 %collective-permute-start.8 = (f32[8,32,128]{2,1,0:T(8,128)S(1)}, f32[8,32,128]{2,1,0:T(8,128)S(1)}, u32[]{:S(2)}, u32[]{:S(2)}) collective-permute-start(f32[8,32,128]{2,1,0:T(8,128)S(1)} %get-tuple-element.91), channel_id=1, source_target_pairs={{4,8},{0,12},{8,4},{12,0},{5,9},{1,13},{9,5},{13,1},{6,10},{2,14},... | collective-permute-start | bytes 393224 | tf_op jit(solution)/shard_map/ppermute | solution.py:119
  35.1 8.4 %collective-permute-start.13 = (f32[16,32,128]{2,1,0:T(8,128)S(1)}, f32[16,32,128]{2,1,0:T(8,128)S(1)}, u32[]{:S(2)}, u32[]{:S(2)}) collective-permute-start(f32[16,32,128]{2,1,0:T(8,128)S(1)} %add.47), channel_id=1, source_target_pairs={{0,2},{1,3},{2,0},{3,1},{4,6},{5,7},{6,4},{7,5},{8,10},{9,11},{10,... | collective-permute-start | bytes 786440 | tf_op jit(solution)/shard_map/ppermute | solution.py:502
  43.6 1.7 %collective-permute-start.14 = (f32[16,32,128]{2,1,0:T(8,128)S(1)}, f32[16,32,128]{2,1,0:T(8,128)S(1)}, u32[]{:S(2)}, u32[]{:S(2)}) collective-permute-start(f32[16,32,128]{2,1,0:T(8,128)S(1)} %add.49.refs_3_), channel_id=1, source_target_pairs={{0,1},{1,0},{2,3},{3,2},{4,5},{5,4},{6,7},{7,6},{8,9},{9,8},{10,11... | collective-permute-start | bytes 786440 | tf_op jit(solution)/shard_map/ppermute | solution.py:564
  44.7 2.5 %collective-permute-start.12 = (f32[16,32,128]{2,1,0:T(8,128)S(1)}, f32[16,32,128]{2,1,0:T(8,128)S(1)}, u32[]{:S(2)}, u32[]{:S(2)}) collective-permute-start(f32[16,32,128]{2,1,0:T(8,128)S(1)} %get-tuple-element.99), channel_id=1, source_target_pairs={{0,1},{1,0},{2,3},{3,2},{4,5},{5,4},{6,7},{7,6},{8,9},{9,8},{10,11... | collective-permute-start | bytes 786440 | tf_op jit(solution)/shard_map/ppermute | solution.py:568
  46.7 12.7 %collective-permute-start.17 = (f32[8,32,128]{2,1,0:T(8,128)S(1)}, f32[8,32,128]{2,1,0:T(8,128)S(1)}, u32[]{:S(2)}, u32[]{:S(2)}) collective-permute-start(f32[8,32,128]{2,1,0:T(8,128)S(1)} %get-tuple-element.105), channel_id=1, source_target_pairs={{0,8},{4,12},{8,0},{12,4},{1,9},{5,13},{9,1},{13,5},{2,10},{6,14},... | collective-permute-start | bytes 393224 | tf_op jit(solution)/shard_map/ppermute | solution.py:119
  47.3 14.1 %collective-permute-start.15 = (f32[16,32,128]{2,1,0:T(8,128)S(1)}, f32[16,32,128]{2,1,0:T(8,128)S(1)}, u32[]{:S(2)}, u32[]{:S(2)}) collective-permute-start(f32[16,32,128]{2,1,0:T(8,128)S(1)} %add.50), channel_id=1, source_target_pairs={{0,2},{1,3},{2,0},{3,1},{4,6},{5,7},{6,4},{7,5},{8,10},{9,11},{10,... | collective-permute-start | bytes 786440 | tf_op jit(solution)/shard_map/ppermute | solution.py:502
  50.5 9.9 %collective-permute-start.16 = (f32[8,32,128]{2,1,0:T(8,128)S(1)}, f32[8,32,128]{2,1,0:T(8,128)S(1)}, u32[]{:S(2)}, u32[]{:S(2)}) collective-permute-start(f32[8,32,128]{2,1,0:T(8,128)S(1)} %get-tuple-element.104), channel_id=1, source_target_pairs={{4,8},{0,12},{8,4},{12,0},{5,9},{1,13},{9,5},{13,1},{6,10},{2,14},... | collective-permute-start | bytes 393224 | tf_op jit(solution)/shard_map/ppermute | solution.py:119
  53.7 7.9 %collective-permute-start.19 = (f32[8,32,128]{2,1,0:T(8,128)S(1)}, f32[8,32,128]{2,1,0:T(8,128)S(1)}, u32[]{:S(2)}, u32[]{:S(2)}) collective-permute-start(f32[8,32,128]{2,1,0:T(8,128)S(1)} %get-tuple-element.109), channel_id=1, source_target_pairs={{0,4},{8,12},{4,0},{12,8},{1,5},{9,13},{5,1},{13,9},{2,6},{10,14},... | collective-permute-start | bytes 393224 | tf_op jit(solution)/shard_map/ppermute | solution.py:119
  61.4 1.7 %collective-permute-start.18 = (f32[16,32,128]{2,1,0:T(8,128)S(1)}, f32[16,32,128]{2,1,0:T(8,128)S(1)}, u32[]{:S(2)}, u32[]{:S(2)}) collective-permute-start(f32[16,32,128]{2,1,0:T(8,128)S(1)} %add.51.refs_3_), channel_id=1, source_target_pairs={{0,1},{1,0},{2,3},{3,2},{4,5},{5,4},{6,7},{7,6},{8,9},{9,8},{10,11... | collective-permute-start | bytes 786440 | tf_op jit(solution)/shard_map/ppermute | solution.py:574
  62.6 2.6 %collective-permute-start.23 = (f32[16,32,128]{2,1,0:T(8,128)S(1)}, f32[16,32,128]{2,1,0:T(8,128)S(1)}, u32[]{:S(2)}, u32[]{:S(2)}) collective-permute-start(f32[16,32,128]{2,1,0:T(8,128)S(1)} %get-tuple-element.118), channel_id=1, source_target_pairs={{0,1},{1,0},{2,3},{3,2},{4,5},{5,4},{6,7},{7,6},{8,9},{9,8},{10,11... | collective-permute-start | bytes 786440 | tf_op jit(solution)/shard_map/ppermute | solution.py:578
  64.7 10.8 %collective-permute-start.22 = (f32[8,32,128]{2,1,0:T(8,128)S(1)}, f32[8,32,128]{2,1,0:T(8,128)S(1)}, u32[]{:S(2)}, u32[]{:S(2)}) collective-permute-start(f32[8,32,128]{2,1,0:T(8,128)S(1)} %get-tuple-element.115), channel_id=1, source_target_pairs={{0,8},{4,12},{8,0},{12,4},{1,9},{5,13},{9,1},{13,5},{2,10},{6,14},... | collective-permute-start | bytes 393224 | tf_op jit(solution)/shard_map/ppermute | solution.py:119
  66.2 7.0 %collective-permute-start.24 = (f32[64,128]{1,0:T(8,128)S(1)}, f32[64,128]{1,0:T(8,128)S(1)}, u32[]{:S(2)}, u32[]{:S(2)}) collective-permute-start(f32[64,128]{1,0:T(8,128)S(1)} %cross.1), channel_id=1, source_target_pairs={{0,4},{4,0},{8,12},{12,8},{1,5},{5,1},{9,13},{13,9},{2,6},{6,2},{1... | collective-permute-start | bytes 98312 | tf_op jit(solution)/shard_map/ppermute | solution.py:140
  67.4 14.7 %collective-permute-start.28 = (f32[16,32,128]{2,1,0:T(8,128)S(1)}, f32[16,32,128]{2,1,0:T(8,128)S(1)}, u32[]{:S(2)}, u32[]{:S(2)}) collective-permute-start(f32[16,32,128]{2,1,0:T(8,128)S(1)} %add.52), channel_id=1, source_target_pairs={{0,2},{1,3},{2,0},{3,1},{4,6},{5,7},{6,4},{7,5},{8,10},{9,11},{10,... | collective-permute-start | bytes 786440 | tf_op jit(solution)/shard_map/ppermute | solution.py:502
  68.9 12.1 %collective-permute-start.20 = (f32[8,32,128]{2,1,0:T(8,128)S(1)}, f32[8,32,128]{2,1,0:T(8,128)S(1)}, u32[]{:S(2)}, u32[]{:S(2)}) collective-permute-start(f32[8,32,128]{2,1,0:T(8,128)S(1)} %get-tuple-element.112), channel_id=1, source_target_pairs={{0,4},{8,12},{4,0},{12,8},{1,5},{9,13},{5,1},{13,9},{2,6},{10,14},... | collective-permute-start | bytes 393224 | tf_op jit(solution)/shard_map/ppermute | solution.py:119
  69.8 9.3 %collective-permute-start.21 = (f32[8,32,128]{2,1,0:T(8,128)S(1)}, f32[8,32,128]{2,1,0:T(8,128)S(1)}, u32[]{:S(2)}, u32[]{:S(2)}) collective-permute-start(f32[8,32,128]{2,1,0:T(8,128)S(1)} %get-tuple-element.113), channel_id=1, source_target_pairs={{4,8},{0,12},{8,4},{12,0},{5,9},{1,13},{9,5},{13,1},{6,10},{2,14},... | collective-permute-start | bytes 393224 | tf_op jit(solution)/shard_map/ppermute | solution.py:119
  73.3 7.7 %collective-permute-start.25 = (f32[64,128]{1,0:T(8,128)S(1)}, f32[64,128]{1,0:T(8,128)S(1)}, u32[]{:S(2)}, u32[]{:S(2)}) collective-permute-start(f32[64,128]{1,0:T(8,128)S(1)} %add.53), channel_id=1, source_target_pairs={{0,8},{4,12},{8,0},{12,4},{1,9},{5,13},{9,1},{13,5},{2,10},{6,14},... | collective-permute-start | bytes 98312 | tf_op jit(solution)/shard_map/ppermute | solution.py:149
  82.0 1.6 %collective-permute-start.26 = (f32[16,32,128]{2,1,0:T(8,128)S(1)}, f32[16,32,128]{2,1,0:T(8,128)S(1)}, u32[]{:S(2)}, u32[]{:S(2)}) collective-permute-start(f32[16,32,128]{2,1,0:T(8,128)S(1)} %get-tuple-element.125), channel_id=1, source_target_pairs={{0,1},{1,0},{2,3},{3,2},{4,5},{5,4},{6,7},{7,6},{8,9},{9,8},{10,11... | collective-permute-start | bytes 786440 | tf_op jit(solution)/shard_map/ppermute | solution.py:591
  82.2 7.0 %collective-permute-start.29 = (f32[16,32,128]{2,1,0:T(8,128)S(1)}, f32[16,32,128]{2,1,0:T(8,128)S(1)}, u32[]{:S(2)}, u32[]{:S(2)}) collective-permute-start(f32[16,32,128]{2,1,0:T(8,128)S(1)} %add.56.mine_ref), channel_id=1, source_target_pairs={{0,1},{1,0},{2,3},{3,2},{4,5},{5,4},{6,7},{7,6},{8,9},{9,8},{10,11... | collective-permute-start | bytes 786440 | tf_op jit(solution)/shard_map/ppermute | solution.py:588
  83.7 8.9 %collective-permute-start.27 = (f32[16,32,128]{2,1,0:T(8,128)S(1)}, f32[16,32,128]{2,1,0:T(8,128)S(1)}, u32[]{:S(2)}, u32[]{:S(2)}) collective-permute-start(f32[16,32,128]{2,1,0:T(8,128)S(1)} %add.55), channel_id=1, source_target_pairs={{0,2},{1,3},{2,0},{3,1},{4,6},{5,7},{6,4},{7,5},{8,10},{9,11},{10,... | collective-permute-start | bytes 786440 | tf_op jit(solution)/shard_map/ppermute | solution.py:502
  92.7 1.6 %collective-permute-start.30 = (f32[16,32,128]{2,1,0:T(8,128)S(1)}, f32[16,32,128]{2,1,0:T(8,128)S(1)}, u32[]{:S(2)}, u32[]{:S(2)}) collective-permute-start(f32[16,32,128]{2,1,0:T(8,128)S(1)} %add.57.mine_ref), channel_id=1, source_target_pairs={{0,1},{1,0},{2,3},{3,2},{4,5},{5,4},{6,7},{7,6},{8,9},{9,8},{10,11... | collective-permute-start | bytes 786440 | tf_op jit(solution)/shard_map/ppermute | solution.py:599
  96.3 4.0 %collective-permute-start.31 = (f32[72,128]{1,0:T(8,128)S(1)}, f32[72,128]{1,0:T(8,128)S(1)}, u32[]{:S(2)}, u32[]{:S(2)}) collective-permute-start(f32[72,128]{1,0:T(8,128)S(1)} %get-tuple-element.138), channel_id=1, source_target_pairs={{0,4},{4,0},{8,12},{12,8},{1,5},{5,1},{9,13},{13,9},{2,6},{6,2},{1... | collective-permute-start | bytes 110600 | tf_op jit(solution)/shard_map/ppermute | solution.py:140
  100.3 4.9 %collective-permute-start.32 = (f32[72,128]{1,0:T(8,128)S(1)}, f32[72,128]{1,0:T(8,128)S(1)}, u32[]{:S(2)}, u32[]{:S(2)}) collective-permute-start(f32[72,128]{1,0:T(8,128)S(1)} %add.58), channel_id=1, source_target_pairs={{0,8},{4,12},{8,0},{12,4},{1,9},{5,13},{9,1},{13,5},{2,10},{6,14},... | collective-permute-start | bytes 110600 | tf_op jit(solution)/shard_map/ppermute | solution.py:149
  (5 other events, 29.2 us)

commit v10 on v9

--- a/solution.py
+++ b/solution.py
@@ -568,25 +568,26 @@
     core = lax.ppermute(give_b, "vec", swap)
     mine_b = keep_b + after(core, y_a)
     (acc_a,) = own(y_a, after(acc_a, mine_b))
-    acc_a = join(acc_a, got_a, groups[2])
-    acc_a = join(acc_a, got_a, groups[1])
     mine_b = across(mine_b, acc_a)
     other_b = lax.ppermute(mine_b, "vec", swap)
+    acc_a = join(after(acc_a, mine_b), got_a, groups[2])
+    y_b, acc_b, got_b = resend(mine_b, after(other_b, acc_a))
+    acc_a = join(after(acc_a, y_b), got_a, groups[1])
     keep_a, give_a = join(acc_a, got_a, groups[0], last=True)
-    y_b, acc_b, got_b = resend(mine_b, after(other_b, keep_a))
 
     core = lax.ppermute(give_a, "vec", swap)
-    mine_a = keep_a + after(core, y_b)
+    acc_b = join(acc_b, got_b, groups[0])
+    mine_a = keep_a + after(core, acc_b)
     (gram,) = call(cross_body, [(width, 2 * width)], [VMEM] * 3, name="cross")(x, y_a, after(y_b, mine_a))
     cross_gram = start_sum(gram, "res")
-    acc_b = join(after(acc_b, cross_gram), got_b, groups[2])
-    (acc_b,) = own(y_b, acc_b)
+    (acc_b,) = own(y_b, after(acc_b, gram))
+    acc_b = after(acc_b, cross_gram)
     acc_b = join(acc_b, got_b, groups[1])
     cross_gram = end_sum(cross_gram, "res", acc_b)
     acc_b = after(acc_b, cross_gram)
     mine_a = across(mine_a, acc_b)
     other_a = lax.ppermute(mine_a, "vec", swap)
-    keep_b, give_b = join(acc_b, got_b, groups[0], last=True)
+    keep_b, give_b = join(acc_b, got_b, groups[2], last=True)
 
     core = lax.ppermute(give_b, "vec", swap)
     mine_b = keep_b + core

time: 111 us -> 110 us (level)
  starting transfers between devices: 38.8 us -> 36.2 us
  waiting for transfers between devices: 26.3 us -> 28.1 us
    ppermute x3, waiting for transfers between devices: 7.25 us -> 10 us  [end_sum(): got = lax.ppermute(block, axis, [(i, i ^ step) for i in range(size)])]
    ppermute x15, starting transfers between devices: 26.5 us -> 25.2 us  [exchange(): lax.ppermute(block, axis, [(a, b) for a, b in pairs] + [(b, a) for a, b i...]
where the time goes in v10:
time: 110 us
  Pallas kernels  43.4 us (39%)
  starting transfers between devices  36.2 us (33%)
  waiting for transfers between devices  28.1 us (26%)
    ppermute x15, starting transfers between devices, exchange(): lax.ppermute(block, axis, [(a, b) for a, b in pairs] + [(b, a) for a, b i...  25.2 us
    pallas_call x12, Pallas kernels, join(): call(body, [halfchunk] * 2 if last else [chunk], [SMEM] * (3 + size) + [V...  11.9 us
    ppermute x15, waiting for transfers between devices, exchange(): lax.ppermute(block, axis, [(a, b) for a, b in pairs] + [(b, a) for a, b i...  11.5 us
    ppermute x3, waiting for transfers between devices, end_sum(): got = lax.ppermute(block, axis, [(i, i ^ step) for i in range(size)])  10 us
    pallas_call x3, Pallas kernels, own(): call(own_body, [chunk] * len(accs), [SMEM] * 2 + [VMEM] * (2 + len(accs))...  5.46 us
    ppermute x4, starting transfers between devices, across(): got = lax.ppermute(mine, 'vec', [(i, i ^ step) for i in range(lanes)])  5.21 us
    pallas_call x1, Pallas kernels, local(): call(second_body, [square, square, (2 * width, 3 * width), square], [VMEM...  3.94 us
    pallas_call x1, Pallas kernels, local(): call(fourth_body, [square, square, (width, 2 * width)], [VMEM], name='fou...  3.7 us
  transfers between devices with their start and end apart: 33, of which 13 were waited for; matrix products, arithmetic and copies ran while one was open for 1% of the time, Pallas kernels for 31%

profile of v10, /device:TPU:0, one launch (start us, length us, event | category | flops | bytes accessed | tf_op | source)
XLA Modules:
  0.0 110.0 jit_solution(3282925120073089071)
XLA Ops:
  0.6 5.1 %collective-permute-start.2 = (s32[1,1,44]{2,1,0:T(1,128)}, s32[1,1,44]{2,1,0:T(1,128)S(1)}, u32[]{:S(2)}, u32[]{:S(2)}) collective-permute-start(s32[1,1,44]{2,1,0:T(1,128)} %cols_ref.5), channel_id=1, source_target_pairs={{4,8},{0,12},{8,4},{12,0},{5,9},{1,13},{9,5},{13,1},{6,10},{2,14},... | collective-permute-start | bytes 536 | tf_op jit(solution)/shard_map/ppermute | solution.py:119
  7.2 2.3 %prepare.1 = (f32[32,64,128]{2,1,0:T(8,128)S(1)}, bf16[44,2,128,128]{3,2,1,0:T(8,128)(2,1)S(1)}, f32[32,32,128]{2,1,0:T(8,128)S(1)}, f32[32,32,128]{2,1,0:T(8,128)S(1)}) custom-call(f32[32,64,128]{2,1,0:T(8,128)} %x_hbm.1, f32[32,128]{1,0:T(8,128)} %refs_5_.3, f32[1,1,44,128,128]{4,3,2,1,0:T(8,128)} %tiles_hbm.1), custom_call_target="tpu_custom_call" | custom-call | tf_op jit(solution)/shard_map/prepare/pallas_call | solution.py:526
  11.8 1.8 %collective-permute-start.5 = (f32[8,32,128]{2,1,0:T(8,128)S(1)}, f32[8,32,128]{2,1,0:T(8,128)S(1)}, u32[]{:S(2)}, u32[]{:S(2)}) collective-permute-start(f32[8,32,128]{2,1,0:T(8,128)S(1)} %get-tuple-element.81), channel_id=1, source_target_pairs={{0,4},{8,12},{4,0},{12,8},{1,5},{9,13},{5,1},{13,9},{2,6},{10,14},... | collective-permute-start | bytes 393224 | tf_op jit(solution)/shard_map/ppermute | solution.py:119
  14.6 1.6 %collective-permute-start.4 = (f32[8,32,128]{2,1,0:T(8,128)S(1)}, f32[8,32,128]{2,1,0:T(8,128)S(1)}, u32[]{:S(2)}, u32[]{:S(2)}) collective-permute-start(f32[8,32,128]{2,1,0:T(8,128)S(1)} %get-tuple-element.80), channel_id=1, source_target_pairs={{4,8},{0,12},{8,4},{12,0},{5,9},{1,13},{9,5},{13,1},{6,10},{2,14},... | collective-permute-start | bytes 393224 | tf_op jit(solution)/shard_map/ppermute | solution.py:119
  16.2 2.0 %own.3 = (f32[32,32,128]{2,1,0:T(8,128)S(1)}, f32[32,32,128]{2,1,0:T(8,128)S(1)}) custom-call(s32[1,1,44]{2,1,0:T(1,128)S(1)} %copy-done.1, s32[1,1,44]{2,1,0:T(1,128)S(1)} %copy-done.2, f32[32,64,128]{2,1,0:T(8,128)S(1)} %get-tuple-element.118.refs_3_.x_ref, ...), custom_call_target="tpu_custom_call", output_to_operand_aliasing={{0}: (4, {}), {1}: (5, {})} | custom-call | tf_op jit(solution)/shard_map/own/pallas_call | solution.py:517
  19.8 1.5 %collective-permute-start.6 = (f32[64,64]{1,0:T(8,128)S(1)}, f32[64,64]{1,0:T(8,128)S(1)}, u32[]{:S(2)}, u32[]{:S(2)}) collective-permute-start(f32[64,64]{1,0:T(8,128)S(1)} %gram.1), channel_id=1, source_target_pairs={{0,4},{4,0},{8,12},{12,8},{1,5},{5,1},{9,13},{13,9},{2,6},{6,2},{1... | collective-permute-start | bytes 49160 | tf_op jit(solution)/shard_map/ppermute | solution.py:140
  21.2 1.7 %collective-permute-done.4.refs_1_ = f32[8,32,128]{2,1,0:T(8,128)S(1)} collective-permute-done((f32[8,32,128]{2,1,0:T(8,128)S(1)}, f32[8,32,128]{2,1,0:T(8,128)S(1)}, u32[]{:S(2)}, u32[]{:S(2)}) %collective-permute-start.4) | collective-permute-done | bytes 131104 | tf_op jit(solution)/shard_map/ppermute | solution.py:119
  23.9 3.9 %collective-permute-start.9 = (f32[8,32,128]{2,1,0:T(8,128)S(1)}, f32[8,32,128]{2,1,0:T(8,128)S(1)}, u32[]{:S(2)}, u32[]{:S(2)}) collective-permute-start(f32[8,32,128]{2,1,0:T(8,128)S(1)} %get-tuple-element.95), channel_id=1, source_target_pairs={{0,4},{8,12},{4,0},{12,8},{1,5},{9,13},{5,1},{13,9},{2,6},{10,14},... | collective-permute-start | bytes 393224 | tf_op jit(solution)/shard_map/ppermute | solution.py:119
  29.0 2.6 %collective-permute-start.7 = (f32[8,32,128]{2,1,0:T(8,128)S(1)}, f32[8,32,128]{2,1,0:T(8,128)S(1)}, u32[]{:S(2)}, u32[]{:S(2)}) collective-permute-start(f32[8,32,128]{2,1,0:T(8,128)S(1)} %get-tuple-element.92), channel_id=1, source_target_pairs={{0,8},{4,12},{8,0},{12,4},{1,9},{5,13},{9,1},{13,5},{2,10},{6,14},... | collective-permute-start | bytes 393224 | tf_op jit(solution)/shard_map/ppermute | solution.py:119
  31.6 1.9 %collective-permute-start.8 = (f32[8,32,128]{2,1,0:T(8,128)S(1)}, f32[8,32,128]{2,1,0:T(8,128)S(1)}, u32[]{:S(2)}, u32[]{:S(2)}) collective-permute-start(f32[8,32,128]{2,1,0:T(8,128)S(1)} %get-tuple-element.94), channel_id=1, source_target_pairs={{4,8},{0,12},{8,4},{12,0},{5,9},{1,13},{9,5},{13,1},{6,10},{2,14},... | collective-permute-start | bytes 393224 | tf_op jit(solution)/shard_map/ppermute | solution.py:119
  35.0 1.6 %collective-permute-start.13 = (f32[16,32,128]{2,1,0:T(8,128)S(1)}, f32[16,32,128]{2,1,0:T(8,128)S(1)}, u32[]{:S(2)}, u32[]{:S(2)}) collective-permute-start(f32[16,32,128]{2,1,0:T(8,128)S(1)} %add.47), channel_id=1, source_target_pairs={{0,2},{1,3},{2,0},{3,1},{4,6},{5,7},{6,4},{7,5},{8,10},{9,11},{10,... | collective-permute-start | bytes 786440 | tf_op jit(solution)/shard_map/ppermute | solution.py:502
  36.5 2.5 %collective-permute-done.10 = f32[64,64]{1,0:T(8,128)S(1)} collective-permute-done((f32[64,64]{1,0:T(8,128)S(1)}, f32[64,64]{1,0:T(8,128)S(1)}, u32[]{:S(2)}, u32[]{:S(2)}) %collective-permute-start.10) | collective-permute-done | bytes 16416 | tf_op jit(solution)/shard_map/ppermute | solution.py:149
  39.0 3.0 %first.1.inverse_ref = f32[64,64]{1,0:T(8,128)S(1)} custom-call(f32[64,64]{1,0:T(8,128)S(1)} %add.48.gram_ref), custom_call_target="tpu_custom_call" | custom-call | tf_op jit(solution)/shard_map/first/pallas_call | solution.py:561
  45.1 1.4 %resend.2 = (f32[32,32,128]{2,1,0:T(8,128)S(1)}, f32[32,32,128]{2,1,0:T(8,128)S(1)}, f32[8,32,128]{2,1,0:T(8,128)S(1)}, f32[8,32,128]{2,1,0:T(8,128)S(1)}, f32[8,32,128]{2,1,0:T(8,128)S(1)}) custom-call(s32[4]{0:T(128)S(1)} %pad_add_fusion.place_ref, s32[1,1,44]{2,1,0:T(1,128)S(1)} %copy-done.1, s32[1,1,3]{2,1,0:T(1,128)S(1)} %copy-done.3, ...), custom_call_target="tpu_custom_call" | custom-call | tf_op jit(solution)/shard_map/resend/pallas_call | solution.py:508
  46.6 1.6 %collective-permute-start.15 = (f32[16,32,128]{2,1,0:T(8,128)S(1)}, f32[16,32,128]{2,1,0:T(8,128)S(1)}, u32[]{:S(2)}, u32[]{:S(2)}) collective-permute-start(f32[16,32,128]{2,1,0:T(8,128)S(1)} %add.50), channel_id=1, source_target_pairs={{0,2},{1,3},{2,0},{3,1},{4,6},{5,7},{6,4},{7,5},{8,10},{9,11},{10,... | collective-permute-start | bytes 786440 | tf_op jit(solution)/shard_map/ppermute | solution.py:502
  48.6 1.7 %own.4.refs_3_ = f32[32,32,128]{2,1,0:T(8,128)S(1)} custom-call(s32[1,1,44]{2,1,0:T(1,128)S(1)} %copy-done.1, s32[1,1,44]{2,1,0:T(1,128)S(1)} %copy-done.2, f32[32,32,128]{2,1,0:T(8,128)S(1)} %get-tuple-element.105.x_ref.a_ref, bf16[44,2,128,128]{3,2,1,0:T(8,128)(2,1)S(1)} %get-tuple-element.77.refs_4_.split_ref.refs_2_.refs_6_, ...), custom_call_target="tpu_custom_call", output_to_operand_aliasing={{}: (4, {})} | custom-call | tf_op jit(solution)/shard_map/own/pallas_call | solution.py:517
  50.4 1.5 %collective-permute-start.21 = (f32[8,32,128]{2,1,0:T(8,128)S(1)}, f32[8,32,128]{2,1,0:T(8,128)S(1)}, u32[]{:S(2)}, u32[]{:S(2)}) collective-permute-start(f32[8,32,128]{2,1,0:T(8,128)S(1)} %get-tuple-element.119), channel_id=1, source_target_pairs={{0,4},{8,12},{4,0},{12,8},{1,5},{9,13},{5,1},{13,9},{2,6},{10,14},... | collective-permute-start | bytes 393224 | tf_op jit(solution)/shard_map/ppermute | solution.py:119
  51.9 2.5 %collective-permute-start.22 = (f32[8,32,128]{2,1,0:T(8,128)S(1)}, f32[8,32,128]{2,1,0:T(8,128)S(1)}, u32[]{:S(2)}, u32[]{:S(2)}) collective-permute-start(f32[8,32,128]{2,1,0:T(8,128)S(1)} %get-tuple-element.120), channel_id=1, source_target_pairs={{4,8},{0,12},{8,4},{12,0},{5,9},{1,13},{9,5},{13,1},{6,10},{2,14},... | collective-permute-start | bytes 393224 | tf_op jit(solution)/shard_map/ppermute | solution.py:119
  55.1 3.8 %collective-permute-done.17.refs_1_ = f32[8,32,128]{2,1,0:T(8,128)S(1)} collective-permute-done((f32[8,32,128]{2,1,0:T(8,128)S(1)}, f32[8,32,128]{2,1,0:T(8,128)S(1)}, u32[]{:S(2)}, u32[]{:S(2)}) %collective-permute-start.17) | collective-permute-done | bytes 131104 | tf_op jit(solution)/shard_map/ppermute | solution.py:119
  63.5 5.2 %collective-permute-done.20.refs_1_ = f32[8,32,128]{2,1,0:T(8,128)S(1)} collective-permute-done((f32[8,32,128]{2,1,0:T(8,128)S(1)}, f32[8,32,128]{2,1,0:T(8,128)S(1)}, u32[]{:S(2)}, u32[]{:S(2)}) %collective-permute-start.20) | collective-permute-done | bytes 131104 | tf_op jit(solution)/shard_map/ppermute | solution.py:119
  71.0 2.1 %collective-permute-start.18 = (f32[8,32,128]{2,1,0:T(8,128)S(1)}, f32[8,32,128]{2,1,0:T(8,128)S(1)}, u32[]{:S(2)}, u32[]{:S(2)}) collective-permute-start(f32[8,32,128]{2,1,0:T(8,128)S(1)} %get-tuple-element.113), channel_id=1, source_target_pairs={{0,8},{4,12},{8,0},{12,4},{1,9},{5,13},{9,1},{13,5},{2,10},{6,14},... | collective-permute-start | bytes 393224 | tf_op jit(solution)/shard_map/ppermute | solution.py:119
  73.9 1.7 %own.5.refs_3_ = f32[32,32,128]{2,1,0:T(8,128)S(1)} custom-call(s32[1,1,44]{2,1,0:T(1,128)S(1)} %copy-done.1, s32[1,1,44]{2,1,0:T(1,128)S(1)} %copy-done.2, f32[32,32,128]{2,1,0:T(8,128)S(1)} %get-tuple-element.125.b_ref.x_ref, bf16[44,2,128,128]{3,2,1,0:T(8,128)(2,1)S(1)} %get-tuple-element.77.refs_4_.split_ref.refs_2_.refs_6_, ...), custom_call_target="tpu_custom_call", output_to_operand_aliasing={{}: (4, {})} | custom-call | tf_op jit(solution)/shard_map/own/pallas_call | solution.py:517
  77.3 3.2 %collective-permute-done.25 = f32[64,128]{1,0:T(8,128)S(1)} collective-permute-done((f32[64,128]{1,0:T(8,128)S(1)}, f32[64,128]{1,0:T(8,128)S(1)}, u32[]{:S(2)}, u32[]{:S(2)}) %collective-permute-start.25) | collective-permute-done | bytes 32800 | tf_op jit(solution)/shard_map/ppermute | solution.py:149
  84.5 3.9 %second.1 = (f32[64,64]{1,0:T(8,128)S(1)}, f32[64,64]{1,0:T(8,128)S(1)}, f32[128,192]{1,0:T(8,128)S(1)}, f32[64,64]{1,0:T(8,128)S(1)}) custom-call(f32[64,128]{1,0:T(8,128)S(1)} %add.54.gram_ref, f32[64,64]{1,0:T(8,128)S(1)} %first.1.inverse_ref), custom_call_target="tpu_custom_call" | custom-call | tf_op jit(solution)/shard_map/second/pallas_call | solution.py:594
  88.4 1.7 %blend.3 = (f32[16,64,128]{2,1,0:T(8,128)S(1)}, f32[16,64,128]{2,1,0:T(8,128)S(1)}, f32[64,64]{1,0:T(8,128)S(1)}) custom-call(s32[4]{0:T(128)S(1)} %pad_add_fusion.place_ref, f32[32,64,128]{2,1,0:T(8,128)S(1)} %get-tuple-element.118.refs_3_.x_ref, f32[32,32,128]{2,1,0:T(8,128)S(1)} %get-tuple-element.105.x_ref.a_ref, ...), custom_call_target="tpu_custom_call" | custom-call | tf_op jit(solution)/shard_map/blend/pallas_call | solution.py:436
  90.1 1.7 %blend.2 = (f32[16,64,128]{2,1,0:T(8,128)S(1)}, f32[16,64,128]{2,1,0:T(8,128)S(1)}, f32[64,64]{1,0:T(8,128)S(1)}) custom-call(s32[4]{0:T(128)S(1)} %pad_add_fusion.place_ref, f32[32,64,128]{2,1,0:T(8,128)S(1)} %get-tuple-element.118.refs_3_.x_ref, f32[32,32,128]{2,1,0:T(8,128)S(1)} %get-tuple-element.105.x_ref.a_ref, ...), custom_call_target="tpu_custom_call" | custom-call | tf_op jit(solution)/shard_map/blend/pallas_call | solution.py:436
  92.0 1.5 %collective-permute-done.30.other_ref = f32[16,32,128]{2,1,0:T(8,128)S(1)} collective-permute-done((f32[16,32,128]{2,1,0:T(8,128)S(1)}, f32[16,32,128]{2,1,0:T(8,128)S(1)}, u32[]{:S(2)}, u32[]{:S(2)}) %collective-permute-start.30) | collective-permute-done | bytes 262176 | tf_op jit(solution)/shard_map/ppermute | solution.py:600
  93.5 2.0 %third.1 = (f32[32,64,128]{2,1,0:T(8,128)S(1)}, f32[72,128]{1,0:T(8,128)S(1)}) custom-call(s32[4]{0:T(128)S(1)} %pad_add_fusion.place_ref, f32[16,32,128]{2,1,0:T(8,128)S(1)} %add.57.mine_ref, f32[16,32,128]{2,1,0:T(8,128)S(1)} %collective-permute-done.30.other_ref, f32[64,64]{1,0:T(8,128)S(1)} %get-tuple-element.138.gain_ref, ...), custom_call_target="tpu_custom_call" | custom-call | tf_op jit(solution)/shard_map/third/pallas_call | solution.py:601
  96.9 2.6 %collective-permute-done.31 = f32[72,128]{1,0:T(8,128)S(1)} collective-permute-done((f32[72,128]{1,0:T(8,128)S(1)}, f32[72,128]{1,0:T(8,128)S(1)}, u32[]{:S(2)}, u32[]{:S(2)}) %collective-permute-start.31) | collective-permute-done | bytes 36896 | tf_op jit(solution)/shard_map/ppermute | solution.py:140
  100.1 4.3 %collective-permute-done.32 = f32[72,128]{1,0:T(8,128)S(1)} collective-permute-done((f32[72,128]{1,0:T(8,128)S(1)}, f32[72,128]{1,0:T(8,128)S(1)}, u32[]{:S(2)}, u32[]{:S(2)}) %collective-permute-start.32) | collective-permute-done | bytes 36896 | tf_op jit(solution)/shard_map/ppermute | solution.py:149
  104.4 3.7 %fourth.1 = (f32[64,64]{1,0:T(8,128)S(1)}, f32[64,64]{1,0:T(8,128)S(1)}, f32[64,128]{1,0:T(8,128)S(1)}) custom-call(f32[72,128]{1,0:T(8,128)S(1)} %add.59.gram_ref), custom_call_target="tpu_custom_call" | custom-call | tf_op jit(solution)/shard_map/fourth/pallas_call | solution.py:609
  108.1 1.9 %last.1 = (f32[32,64,128]{2,1,0:T(8,128)}, f32[4,64,64]{2,1,0:T(8,128)}) custom-call(f32[32,64,128]{2,1,0:T(8,128)S(1)} %get-tuple-element.143.w_ref, f32[16,64,128]{2,1,0:T(8,128)S(1)} %get-tuple-element.141.refs_2_.low_ref, f32[16,64,128]{2,1,0:T(8,128)S(1)} %get-tuple-element.142.refs_3_.high_ref, f32[64,128]{1,0:T(8,128)S(1)} %get-tuple-element.145.coef_ref, ...), custom_call_target="tpu_custom_call" | custom-call | tf_op jit(solution)/shard_map/last/pallas_call | solution.py:612
  (86 shorter events, 29.4 us)
Async XLA Ops:
  0.6 8.8 %collective-permute-start.2 = (s32[1,1,44]{2,1,0:T(1,128)}, s32[1,1,44]{2,1,0:T(1,128)S(1)}, u32[]{:S(2)}, u32[]{:S(2)}) collective-permute-start(s32[1,1,44]{2,1,0:T(1,128)} %cols_ref.5), channel_id=1, source_target_pairs={{4,8},{0,12},{8,4},{12,0},{5,9},{1,13},{9,5},{13,1},{6,10},{2,14},... | collective-permute-start | bytes 536 | tf_op jit(solution)/shard_map/ppermute | solution.py:119
  5.8 3.7 %collective-permute-start.1 = (s32[1,1,44]{2,1,0:T(1,128)}, s32[1,1,44]{2,1,0:T(1,128)S(1)}, u32[]{:S(2)}, u32[]{:S(2)}) collective-permute-start(s32[1,1,44]{2,1,0:T(1,128)} %cols_ref.5), channel_id=1, source_target_pairs={{0,4},{8,12},{4,0},{12,8},{1,5},{9,13},{5,1},{13,9},{2,6},{10,14},... | collective-permute-start | bytes 536 | tf_op jit(solution)/shard_map/ppermute | solution.py:119
  5.8 4.6 %collective-permute-start = (s32[1,1,44]{2,1,0:T(1,128)}, s32[1,1,44]{2,1,0:T(1,128)S(1)}, u32[]{:S(2)}, u32[]{:S(2)}) collective-permute-start(s32[1,1,44]{2,1,0:T(1,128)} %cols_ref.5), channel_id=1, source_target_pairs={{0,8},{4,12},{8,0},{12,4},{1,9},{5,13},{9,1},{13,5},{2,10},{6,14},... | collective-permute-start | bytes 536 | tf_op jit(solution)/shard_map/ppermute | solution.py:119
  11.8 6.5 %collective-permute-start.5 = (f32[8,32,128]{2,1,0:T(8,128)S(1)}, f32[8,32,128]{2,1,0:T(8,128)S(1)}, u32[]{:S(2)}, u32[]{:S(2)}) collective-permute-start(f32[8,32,128]{2,1,0:T(8,128)S(1)} %get-tuple-element.81), channel_id=1, source_target_pairs={{0,4},{8,12},{4,0},{12,8},{1,5},{9,13},{5,1},{13,9},{2,6},{10,14},... | collective-permute-start | bytes 393224 | tf_op jit(solution)/shard_map/ppermute | solution.py:119
  13.6 14.3 %collective-permute-start.3 = (f32[8,32,128]{2,1,0:T(8,128)S(1)}, f32[8,32,128]{2,1,0:T(8,128)S(1)}, u32[]{:S(2)}, u32[]{:S(2)}) collective-permute-start(f32[8,32,128]{2,1,0:T(8,128)S(1)} %get-tuple-element.79), channel_id=1, source_target_pairs={{0,8},{4,12},{8,0},{12,4},{1,9},{5,13},{9,1},{13,5},{2,10},{6,14},... | collective-permute-start | bytes 393224 | tf_op jit(solution)/shard_map/ppermute | solution.py:119
  14.6 8.3 %collective-permute-start.4 = (f32[8,32,128]{2,1,0:T(8,128)S(1)}, f32[8,32,128]{2,1,0:T(8,128)S(1)}, u32[]{:S(2)}, u32[]{:S(2)}) collective-permute-start(f32[8,32,128]{2,1,0:T(8,128)S(1)} %get-tuple-element.80), channel_id=1, source_target_pairs={{4,8},{0,12},{8,4},{12,0},{5,9},{1,13},{9,5},{13,1},{6,10},{2,14},... | collective-permute-start | bytes 393224 | tf_op jit(solution)/shard_map/ppermute | solution.py:119
  19.8 8.0 %collective-permute-start.6 = (f32[64,64]{1,0:T(8,128)S(1)}, f32[64,64]{1,0:T(8,128)S(1)}, u32[]{:S(2)}, u32[]{:S(2)}) collective-permute-start(f32[64,64]{1,0:T(8,128)S(1)} %gram.1), channel_id=1, source_target_pairs={{0,4},{4,0},{8,12},{12,8},{1,5},{5,1},{9,13},{13,9},{2,6},{6,2},{1... | collective-permute-start | bytes 49160 | tf_op jit(solution)/shard_map/ppermute | solution.py:140
  23.9 9.5 %collective-permute-start.9 = (f32[8,32,128]{2,1,0:T(8,128)S(1)}, f32[8,32,128]{2,1,0:T(8,128)S(1)}, u32[]{:S(2)}, u32[]{:S(2)}) collective-permute-start(f32[8,32,128]{2,1,0:T(8,128)S(1)} %get-tuple-element.95), channel_id=1, source_target_pairs={{0,4},{8,12},{4,0},{12,8},{1,5},{9,13},{5,1},{13,9},{2,6},{10,14},... | collective-permute-start | bytes 393224 | tf_op jit(solution)/shard_map/ppermute | solution.py:119
  27.8 11.2 %collective-permute-start.10 = (f32[64,64]{1,0:T(8,128)S(1)}, f32[64,64]{1,0:T(8,128)S(1)}, u32[]{:S(2)}, u32[]{:S(2)}) collective-permute-start(f32[64,64]{1,0:T(8,128)S(1)} %add.46), channel_id=1, source_target_pairs={{0,8},{4,12},{8,0},{12,4},{1,9},{5,13},{9,1},{13,5},{2,10},{6,14},... | collective-permute-start | bytes 49160 | tf_op jit(solution)/shard_map/ppermute | solution.py:149
  29.0 14.5 %collective-permute-start.7 = (f32[8,32,128]{2,1,0:T(8,128)S(1)}, f32[8,32,128]{2,1,0:T(8,128)S(1)}, u32[]{:S(2)}, u32[]{:S(2)}) collective-permute-start(f32[8,32,128]{2,1,0:T(8,128)S(1)} %get-tuple-element.92), channel_id=1, source_target_pairs={{0,8},{4,12},{8,0},{12,4},{1,9},{5,13},{9,1},{13,5},{2,10},{6,14},... | collective-permute-start | bytes 393224 | tf_op jit(solution)/shard_map/ppermute | solution.py:119
  31.6 10.5 %collective-permute-start.8 = (f32[8,32,128]{2,1,0:T(8,128)S(1)}, f32[8,32,128]{2,1,0:T(8,128)S(1)}, u32[]{:S(2)}, u32[]{:S(2)}) collective-permute-start(f32[8,32,128]{2,1,0:T(8,128)S(1)} %get-tuple-element.94), channel_id=1, source_target_pairs={{4,8},{0,12},{8,4},{12,0},{5,9},{1,13},{9,5},{13,1},{6,10},{2,14},... | collective-permute-start | bytes 393224 | tf_op jit(solution)/shard_map/ppermute | solution.py:119
  35.0 8.4 %collective-permute-start.13 = (f32[16,32,128]{2,1,0:T(8,128)S(1)}, f32[16,32,128]{2,1,0:T(8,128)S(1)}, u32[]{:S(2)}, u32[]{:S(2)}) collective-permute-start(f32[16,32,128]{2,1,0:T(8,128)S(1)} %add.47), channel_id=1, source_target_pairs={{0,2},{1,3},{2,0},{3,1},{4,6},{5,7},{6,4},{7,5},{8,10},{9,11},{10,... | collective-permute-start | bytes 786440 | tf_op jit(solution)/shard_map/ppermute | solution.py:502
  43.4 1.7 %collective-permute-start.14 = (f32[16,32,128]{2,1,0:T(8,128)S(1)}, f32[16,32,128]{2,1,0:T(8,128)S(1)}, u32[]{:S(2)}, u32[]{:S(2)}) collective-permute-start(f32[16,32,128]{2,1,0:T(8,128)S(1)} %add.49.refs_3_), channel_id=1, source_target_pairs={{0,1},{1,0},{2,3},{3,2},{4,5},{5,4},{6,7},{7,6},{8,9},{9,8},{10,11... | collective-permute-start | bytes 786440 | tf_op jit(solution)/shard_map/ppermute | solution.py:564
  44.6 2.0 %collective-permute-start.12 = (f32[16,32,128]{2,1,0:T(8,128)S(1)}, f32[16,32,128]{2,1,0:T(8,128)S(1)}, u32[]{:S(2)}, u32[]{:S(2)}) collective-permute-start(f32[16,32,128]{2,1,0:T(8,128)S(1)} %get-tuple-element.102), channel_id=1, source_target_pairs={{0,1},{1,0},{2,3},{3,2},{4,5},{5,4},{6,7},{7,6},{8,9},{9,8},{10,11... | collective-permute-start | bytes 786440 | tf_op jit(solution)/shard_map/ppermute | solution.py:568
  46.6 8.3 %collective-permute-start.15 = (f32[16,32,128]{2,1,0:T(8,128)S(1)}, f32[16,32,128]{2,1,0:T(8,128)S(1)}, u32[]{:S(2)}, u32[]{:S(2)}) collective-permute-start(f32[16,32,128]{2,1,0:T(8,128)S(1)} %add.50), channel_id=1, source_target_pairs={{0,2},{1,3},{2,0},{3,1},{4,6},{5,7},{6,4},{7,5},{8,10},{9,11},{10,... | collective-permute-start | bytes 786440 | tf_op jit(solution)/shard_map/ppermute | solution.py:502
  48.2 10.7 %collective-permute-start.17 = (f32[8,32,128]{2,1,0:T(8,128)S(1)}, f32[8,32,128]{2,1,0:T(8,128)S(1)}, u32[]{:S(2)}, u32[]{:S(2)}) collective-permute-start(f32[8,32,128]{2,1,0:T(8,128)S(1)} %get-tuple-element.110), channel_id=1, source_target_pairs={{0,8},{4,12},{8,0},{12,4},{1,9},{5,13},{9,1},{13,5},{2,10},{6,14},... | collective-permute-start | bytes 393224 | tf_op jit(solution)/shard_map/ppermute | solution.py:119
  50.4 12.1 %collective-permute-start.21 = (f32[8,32,128]{2,1,0:T(8,128)S(1)}, f32[8,32,128]{2,1,0:T(8,128)S(1)}, u32[]{:S(2)}, u32[]{:S(2)}) collective-permute-start(f32[8,32,128]{2,1,0:T(8,128)S(1)} %get-tuple-element.119), channel_id=1, source_target_pairs={{0,4},{8,12},{4,0},{12,8},{1,5},{9,13},{5,1},{13,9},{2,6},{10,14},... | collective-permute-start | bytes 393224 | tf_op jit(solution)/shard_map/ppermute | solution.py:119
  51.9 9.6 %collective-permute-start.22 = (f32[8,32,128]{2,1,0:T(8,128)S(1)}, f32[8,32,128]{2,1,0:T(8,128)S(1)}, u32[]{:S(2)}, u32[]{:S(2)}) collective-permute-start(f32[8,32,128]{2,1,0:T(8,128)S(1)} %get-tuple-element.120), channel_id=1, source_target_pairs={{4,8},{0,12},{8,4},{12,0},{5,9},{1,13},{9,5},{13,1},{6,10},{2,14},... | collective-permute-start | bytes 393224 | tf_op jit(solution)/shard_map/ppermute | solution.py:119
  55.0 4.8 %collective-permute-start.16 = (f32[16,32,128]{2,1,0:T(8,128)S(1)}, f32[16,32,128]{2,1,0:T(8,128)S(1)}, u32[]{:S(2)}, u32[]{:S(2)}) collective-permute-start(f32[16,32,128]{2,1,0:T(8,128)S(1)} %add.51.refs_3_), channel_id=1, source_target_pairs={{0,1},{1,0},{2,3},{3,2},{4,5},{5,4},{6,7},{7,6},{8,9},{9,8},{10,11... | collective-permute-start | bytes 786440 | tf_op jit(solution)/shard_map/ppermute | solution.py:572
  61.3 15.1 %collective-permute-start.19 = (f32[8,32,128]{2,1,0:T(8,128)S(1)}, f32[8,32,128]{2,1,0:T(8,128)S(1)}, u32[]{:S(2)}, u32[]{:S(2)}) collective-permute-start(f32[8,32,128]{2,1,0:T(8,128)S(1)} %get-tuple-element.114), channel_id=1, source_target_pairs={{4,8},{0,12},{8,4},{12,0},{5,9},{1,13},{9,5},{13,1},{6,10},{2,14},... | collective-permute-start | bytes 393224 | tf_op jit(solution)/shard_map/ppermute | solution.py:119
  61.4 7.3 %collective-permute-start.20 = (f32[8,32,128]{2,1,0:T(8,128)S(1)}, f32[8,32,128]{2,1,0:T(8,128)S(1)}, u32[]{:S(2)}, u32[]{:S(2)}) collective-permute-start(f32[8,32,128]{2,1,0:T(8,128)S(1)} %get-tuple-element.116), channel_id=1, source_target_pairs={{0,4},{8,12},{4,0},{12,8},{1,5},{9,13},{5,1},{13,9},{2,6},{10,14},... | collective-permute-start | bytes 393224 | tf_op jit(solution)/shard_map/ppermute | solution.py:119
  63.4 6.4 %collective-permute-start.23 = (f32[16,32,128]{2,1,0:T(8,128)S(1)}, f32[16,32,128]{2,1,0:T(8,128)S(1)}, u32[]{:S(2)}, u32[]{:S(2)}) collective-permute-start(f32[16,32,128]{2,1,0:T(8,128)S(1)} %get-tuple-element.123), channel_id=1, source_target_pairs={{0,1},{1,0},{2,3},{3,2},{4,5},{5,4},{6,7},{7,6},{8,9},{9,8},{10,11... | collective-permute-start | bytes 786440 | tf_op jit(solution)/shard_map/ppermute | solution.py:578
  70.9 4.8 %collective-permute-start.24 = (f32[64,128]{1,0:T(8,128)S(1)}, f32[64,128]{1,0:T(8,128)S(1)}, u32[]{:S(2)}, u32[]{:S(2)}) collective-permute-start(f32[64,128]{1,0:T(8,128)S(1)} %cross.1), channel_id=1, source_target_pairs={{0,4},{4,0},{8,12},{12,8},{1,5},{5,1},{9,13},{13,9},{2,6},{6,2},{1... | collective-permute-start | bytes 98312 | tf_op jit(solution)/shard_map/ppermute | solution.py:140
  71.0 9.6 %collective-permute-start.18 = (f32[8,32,128]{2,1,0:T(8,128)S(1)}, f32[8,32,128]{2,1,0:T(8,128)S(1)}, u32[]{:S(2)}, u32[]{:S(2)}) collective-permute-start(f32[8,32,128]{2,1,0:T(8,128)S(1)} %get-tuple-element.113), channel_id=1, source_target_pairs={{0,8},{4,12},{8,0},{12,4},{1,9},{5,13},{9,1},{13,5},{2,10},{6,14},... | collective-permute-start | bytes 393224 | tf_op jit(solution)/shard_map/ppermute | solution.py:119
  73.1 8.6 %collective-permute-start.28 = (f32[16,32,128]{2,1,0:T(8,128)S(1)}, f32[16,32,128]{2,1,0:T(8,128)S(1)}, u32[]{:S(2)}, u32[]{:S(2)}) collective-permute-start(f32[16,32,128]{2,1,0:T(8,128)S(1)} %add.52), channel_id=1, source_target_pairs={{0,2},{1,3},{2,0},{3,1},{4,6},{5,7},{6,4},{7,5},{8,10},{9,11},{10,... | collective-permute-start | bytes 786440 | tf_op jit(solution)/shard_map/ppermute | solution.py:502
  75.7 4.9 %collective-permute-start.25 = (f32[64,128]{1,0:T(8,128)S(1)}, f32[64,128]{1,0:T(8,128)S(1)}, u32[]{:S(2)}, u32[]{:S(2)}) collective-permute-start(f32[64,128]{1,0:T(8,128)S(1)} %add.53), channel_id=1, source_target_pairs={{0,8},{4,12},{8,0},{12,4},{1,9},{5,13},{9,1},{13,5},{2,10},{6,14},... | collective-permute-start | bytes 98312 | tf_op jit(solution)/shard_map/ppermute | solution.py:149
  81.6 1.6 %collective-permute-start.26 = (f32[16,32,128]{2,1,0:T(8,128)S(1)}, f32[16,32,128]{2,1,0:T(8,128)S(1)}, u32[]{:S(2)}, u32[]{:S(2)}) collective-permute-start(f32[16,32,128]{2,1,0:T(8,128)S(1)} %get-tuple-element.131), channel_id=1, source_target_pairs={{0,1},{1,0},{2,3},{3,2},{4,5},{5,4},{6,7},{7,6},{8,9},{9,8},{10,11... | collective-permute-start | bytes 786440 | tf_op jit(solution)/shard_map/ppermute | solution.py:592
  81.7 6.7 %collective-permute-start.29 = (f32[16,32,128]{2,1,0:T(8,128)S(1)}, f32[16,32,128]{2,1,0:T(8,128)S(1)}, u32[]{:S(2)}, u32[]{:S(2)}) collective-permute-start(f32[16,32,128]{2,1,0:T(8,128)S(1)} %add.56.mine_ref), channel_id=1, source_target_pairs={{0,1},{1,0},{2,3},{3,2},{4,5},{5,4},{6,7},{7,6},{8,9},{9,8},{10,11... | collective-permute-start | bytes 786440 | tf_op jit(solution)/shard_map/ppermute | solution.py:589
  83.2 8.6 %collective-permute-start.27 = (f32[16,32,128]{2,1,0:T(8,128)S(1)}, f32[16,32,128]{2,1,0:T(8,128)S(1)}, u32[]{:S(2)}, u32[]{:S(2)}) collective-permute-start(f32[16,32,128]{2,1,0:T(8,128)S(1)} %add.55), channel_id=1, source_target_pairs={{0,2},{1,3},{2,0},{3,1},{4,6},{5,7},{6,4},{7,5},{8,10},{9,11},{10,... | collective-permute-start | bytes 786440 | tf_op jit(solution)/shard_map/ppermute | solution.py:502
  91.9 1.6 %collective-permute-start.30 = (f32[16,32,128]{2,1,0:T(8,128)S(1)}, f32[16,32,128]{2,1,0:T(8,128)S(1)}, u32[]{:S(2)}, u32[]{:S(2)}) collective-permute-start(f32[16,32,128]{2,1,0:T(8,128)S(1)} %add.57.mine_ref), channel_id=1, source_target_pairs={{0,1},{1,0},{2,3},{3,2},{4,5},{5,4},{6,7},{7,6},{8,9},{9,8},{10,11... | collective-permute-start | bytes 786440 | tf_op jit(solution)/shard_map/ppermute | solution.py:600
  95.5 4.0 %collective-permute-start.31 = (f32[72,128]{1,0:T(8,128)S(1)}, f32[72,128]{1,0:T(8,128)S(1)}, u32[]{:S(2)}, u32[]{:S(2)}) collective-permute-start(f32[72,128]{1,0:T(8,128)S(1)} %get-tuple-element.144), channel_id=1, source_target_pairs={{0,4},{4,0},{8,12},{12,8},{1,5},{5,1},{9,13},{13,9},{2,6},{6,2},{1... | collective-permute-start | bytes 110600 | tf_op jit(solution)/shard_map/ppermute | solution.py:140
  99.5 4.9 %collective-permute-start.32 = (f32[72,128]{1,0:T(8,128)S(1)}, f32[72,128]{1,0:T(8,128)S(1)}, u32[]{:S(2)}, u32[]{:S(2)}) collective-permute-start(f32[72,128]{1,0:T(8,128)S(1)} %add.58), channel_id=1, source_target_pairs={{0,8},{4,12},{8,0},{12,4},{1,9},{5,13},{9,1},{13,5},{2,10},{6,14},... | collective-permute-start | bytes 110600 | tf_op jit(solution)/shard_map/ppermute | solution.py:149
  (5 other events, 29.4 us)

commit v11 on v10

--- a/solution.py
+++ b/solution.py
@@ -579,18 +579,16 @@
     acc_b = join(acc_b, got_b, groups[0])
     mine_a = keep_a + after(core, acc_b)
     (gram,) = call(cross_body, [(width, 2 * width)], [VMEM] * 3, name="cross")(x, y_a, after(y_b, mine_a))
+    (acc_b,) = own(y_b, after(acc_b, gram))
+    acc_b = join(acc_b, got_b, groups[1])
     cross_gram = start_sum(gram, "res")
-    (acc_b,) = own(y_b, after(acc_b, gram))
-    acc_b = after(acc_b, cross_gram)
-    acc_b = join(acc_b, got_b, groups[1])
-    cross_gram = end_sum(cross_gram, "res", acc_b)
-    acc_b = after(acc_b, cross_gram)
-    mine_a = across(mine_a, acc_b)
+    keep_b, give_b = join(after(acc_b, cross_gram), got_b, groups[2], last=True)
+
+    core = lax.ppermute(give_b, "vec", swap)
+    mine_a = across(mine_a, cross_gram)
     other_a = lax.ppermute(mine_a, "vec", swap)
-    keep_b, give_b = join(acc_b, got_b, groups[2], last=True)
-
-    core = lax.ppermute(give_b, "vec", swap)
-    mine_b = keep_b + core
+    cross_gram = end_sum(cross_gram, "res")
+    mine_b = keep_b + after(core, mine_a, cross_gram)
     cross1, lower1, coef, gain = call(
         second_body, [square, square, (2 * width, 3 * width), square], [VMEM] * 2, name="second"
     )(after(cross_gram, mine_b), start_inv)

time: 110 us -> 112 us (1.018)
    ppermute x15, starting transfers between devices: 25.2 us -> 26.5 us  [exchange(): lax.ppermute(block, axis, [(a, b) for a, b in pairs] + [(b, a) for a, b i...]
  transfers between devices with their start and end apart: 33 -> 33, of which waited for: 13 -> 14; matrix products, arithmetic and copies ran while one was open for 1% -> 1% of each run, Pallas kernels for 31% -> 31%
where the time goes in v11:
time: 112 us; the launch traced here: 111 us
  Pallas kernels  43.4 us (39%)
  starting transfers between devices  37.2 us (33%)
  waiting for transfers between devices  28.6 us (26%)
    ppermute x15, starting transfers between devices, exchange(): lax.ppermute(block, axis, [(a, b) for a, b in pairs] + [(b, a) for a, b i...  26.5 us
    pallas_call x12, Pallas kernels, join(): call(body, [halfchunk] * 2 if last else [chunk], [SMEM] * (3 + size) + [V...  11.9 us
    ppermute x15, waiting for transfers between devices, exchange(): lax.ppermute(block, axis, [(a, b) for a, b in pairs] + [(b, a) for a, b i...  11.6 us
    ppermute x3, waiting for transfers between devices, end_sum(): got = lax.ppermute(block, axis, [(i, i ^ step) for i in range(size)])  10.9 us
    pallas_call x3, Pallas kernels, own(): call(own_body, [chunk] * len(accs), [SMEM] * 2 + [VMEM] * (2 + len(accs))...  5.46 us
    ppermute x4, starting transfers between devices, across(): got = lax.ppermute(mine, 'vec', [(i, i ^ step) for i in range(lanes)])  5 us
    pallas_call x1, Pallas kernels, local(): call(second_body, [square, square, (2 * width, 3 * width), square], [VMEM...  3.94 us
    pallas_call x1, Pallas kernels, local(): call(fourth_body, [square, square, (width, 2 * width)], [VMEM], name='fou...  3.7 us
  transfers between devices with their start and end apart: 33, of which 14 were waited for; matrix products, arithmetic and copies ran while one was open for 1% of the time, Pallas kernels for 31%

profile of v11, /device:TPU:0, one launch (start us, length us, event | category | flops | bytes accessed | tf_op | source)
XLA Modules:
  0.0 111.4 jit_solution(13420492174773217093)
XLA Ops:
  0.6 5.1 %collective-permute-start.2 = (s32[1,1,44]{2,1,0:T(1,128)}, s32[1,1,44]{2,1,0:T(1,128)S(1)}, u32[]{:S(2)}, u32[]{:S(2)}) collective-permute-start(s32[1,1,44]{2,1,0:T(1,128)} %cols_ref.5), channel_id=1, source_target_pairs={{4,8},{0,12},{8,4},{12,0},{5,9},{1,13},{9,5},{13,1},{6,10},{2,14},... | collective-permute-start | bytes 536 | tf_op jit(solution)/shard_map/ppermute | solution.py:119
  7.2 2.3 %prepare.1 = (f32[32,64,128]{2,1,0:T(8,128)S(1)}, bf16[44,2,128,128]{3,2,1,0:T(8,128)(2,1)S(1)}, f32[32,32,128]{2,1,0:T(8,128)S(1)}, f32[32,32,128]{2,1,0:T(8,128)S(1)}) custom-call(f32[32,64,128]{2,1,0:T(8,128)} %x_hbm.1, f32[32,128]{1,0:T(8,128)} %refs_5_.3, f32[1,1,44,128,128]{4,3,2,1,0:T(8,128)} %tiles_hbm.1), custom_call_target="tpu_custom_call" | custom-call | tf_op jit(solution)/shard_map/prepare/pallas_call | solution.py:526
  11.8 1.8 %collective-permute-start.5 = (f32[8,32,128]{2,1,0:T(8,128)S(1)}, f32[8,32,128]{2,1,0:T(8,128)S(1)}, u32[]{:S(2)}, u32[]{:S(2)}) collective-permute-start(f32[8,32,128]{2,1,0:T(8,128)S(1)} %get-tuple-element.80), channel_id=1, source_target_pairs={{0,4},{8,12},{4,0},{12,8},{1,5},{9,13},{5,1},{13,9},{2,6},{10,14},... | collective-permute-start | bytes 393224 | tf_op jit(solution)/shard_map/ppermute | solution.py:119
  14.6 1.6 %collective-permute-start.4 = (f32[8,32,128]{2,1,0:T(8,128)S(1)}, f32[8,32,128]{2,1,0:T(8,128)S(1)}, u32[]{:S(2)}, u32[]{:S(2)}) collective-permute-start(f32[8,32,128]{2,1,0:T(8,128)S(1)} %get-tuple-element.79), channel_id=1, source_target_pairs={{4,8},{0,12},{8,4},{12,0},{5,9},{1,13},{9,5},{13,1},{6,10},{2,14},... | collective-permute-start | bytes 393224 | tf_op jit(solution)/shard_map/ppermute | solution.py:119
  16.2 2.0 %own.3 = (f32[32,32,128]{2,1,0:T(8,128)S(1)}, f32[32,32,128]{2,1,0:T(8,128)S(1)}) custom-call(s32[1,1,44]{2,1,0:T(1,128)S(1)} %copy-done.1, s32[1,1,44]{2,1,0:T(1,128)S(1)} %copy-done.2, f32[32,64,128]{2,1,0:T(8,128)S(1)} %get-tuple-element.117.refs_3_.x_ref, ...), custom_call_target="tpu_custom_call", output_to_operand_aliasing={{0}: (4, {}), {1}: (5, {})} | custom-call | tf_op jit(solution)/shard_map/own/pallas_call | solution.py:517
  19.8 1.5 %collective-permute-start.6 = (f32[64,64]{1,0:T(8,128)S(1)}, f32[64,64]{1,0:T(8,128)S(1)}, u32[]{:S(2)}, u32[]{:S(2)}) collective-permute-start(f32[64,64]{1,0:T(8,128)S(1)} %gram.1), channel_id=1, source_target_pairs={{0,4},{4,0},{8,12},{12,8},{1,5},{5,1},{9,13},{13,9},{2,6},{6,2},{1... | collective-permute-start | bytes 49160 | tf_op jit(solution)/shard_map/ppermute | solution.py:140
  21.2 1.7 %collective-permute-done.4.refs_1_ = f32[8,32,128]{2,1,0:T(8,128)S(1)} collective-permute-done((f32[8,32,128]{2,1,0:T(8,128)S(1)}, f32[8,32,128]{2,1,0:T(8,128)S(1)}, u32[]{:S(2)}, u32[]{:S(2)}) %collective-permute-start.4) | collective-permute-done | bytes 131104 | tf_op jit(solution)/shard_map/ppermute | solution.py:119
  23.9 3.9 %collective-permute-start.9 = (f32[8,32,128]{2,1,0:T(8,128)S(1)}, f32[8,32,128]{2,1,0:T(8,128)S(1)}, u32[]{:S(2)}, u32[]{:S(2)}) collective-permute-start(f32[8,32,128]{2,1,0:T(8,128)S(1)} %get-tuple-element.94), channel_id=1, source_target_pairs={{0,4},{8,12},{4,0},{12,8},{1,5},{9,13},{5,1},{13,9},{2,6},{10,14},... | collective-permute-start | bytes 393224 | tf_op jit(solution)/shard_map/ppermute | solution.py:119
  29.0 2.6 %collective-permute-start.7 = (f32[8,32,128]{2,1,0:T(8,128)S(1)}, f32[8,32,128]{2,1,0:T(8,128)S(1)}, u32[]{:S(2)}, u32[]{:S(2)}) collective-permute-start(f32[8,32,128]{2,1,0:T(8,128)S(1)} %get-tuple-element.91), channel_id=1, source_target_pairs={{0,8},{4,12},{8,0},{12,4},{1,9},{5,13},{9,1},{13,5},{2,10},{6,14},... | collective-permute-start | bytes 393224 | tf_op jit(solution)/shard_map/ppermute | solution.py:119
  31.6 1.9 %collective-permute-start.8 = (f32[8,32,128]{2,1,0:T(8,128)S(1)}, f32[8,32,128]{2,1,0:T(8,128)S(1)}, u32[]{:S(2)}, u32[]{:S(2)}) collective-permute-start(f32[8,32,128]{2,1,0:T(8,128)S(1)} %get-tuple-element.93), channel_id=1, source_target_pairs={{4,8},{0,12},{8,4},{12,0},{5,9},{1,13},{9,5},{13,1},{6,10},{2,14},... | collective-permute-start | bytes 393224 | tf_op jit(solution)/shard_map/ppermute | solution.py:119
  35.0 1.6 %collective-permute-start.13 = (f32[16,32,128]{2,1,0:T(8,128)S(1)}, f32[16,32,128]{2,1,0:T(8,128)S(1)}, u32[]{:S(2)}, u32[]{:S(2)}) collective-permute-start(f32[16,32,128]{2,1,0:T(8,128)S(1)} %add.47), channel_id=1, source_target_pairs={{0,2},{1,3},{2,0},{3,1},{4,6},{5,7},{6,4},{7,5},{8,10},{9,11},{10,... | collective-permute-start | bytes 786440 | tf_op jit(solution)/shard_map/ppermute | solution.py:502
  36.5 2.5 %collective-permute-done.10 = f32[64,64]{1,0:T(8,128)S(1)} collective-permute-done((f32[64,64]{1,0:T(8,128)S(1)}, f32[64,64]{1,0:T(8,128)S(1)}, u32[]{:S(2)}, u32[]{:S(2)}) %collective-permute-start.10) | collective-permute-done | bytes 16416 | tf_op jit(solution)/shard_map/ppermute | solution.py:149
  39.0 3.0 %first.1.inverse_ref = f32[64,64]{1,0:T(8,128)S(1)} custom-call(f32[64,64]{1,0:T(8,128)S(1)} %add.48.gram_ref), custom_call_target="tpu_custom_call" | custom-call | tf_op jit(solution)/shard_map/first/pallas_call | solution.py:561
  46.6 1.6 %collective-permute-start.15 = (f32[16,32,128]{2,1,0:T(8,128)S(1)}, f32[16,32,128]{2,1,0:T(8,128)S(1)}, u32[]{:S(2)}, u32[]{:S(2)}) collective-permute-start(f32[16,32,128]{2,1,0:T(8,128)S(1)} %add.50), channel_id=1, source_target_pairs={{0,2},{1,3},{2,0},{3,1},{4,6},{5,7},{6,4},{7,5},{8,10},{9,11},{10,... | collective-permute-start | bytes 786440 | tf_op jit(solution)/shard_map/ppermute | solution.py:502
  48.6 1.7 %own.4.refs_3_ = f32[32,32,128]{2,1,0:T(8,128)S(1)} custom-call(s32[1,1,44]{2,1,0:T(1,128)S(1)} %copy-done.1, s32[1,1,44]{2,1,0:T(1,128)S(1)} %copy-done.2, f32[32,32,128]{2,1,0:T(8,128)S(1)} %get-tuple-element.104.x_ref.a_ref, bf16[44,2,128,128]{3,2,1,0:T(8,128)(2,1)S(1)} %get-tuple-element.76.refs_4_.split_ref.refs_2_.refs_6_, ...), custom_call_target="tpu_custom_call", output_to_operand_aliasing={{}: (4, {})} | custom-call | tf_op jit(solution)/shard_map/own/pallas_call | solution.py:517
  50.4 1.5 %collective-permute-start.21 = (f32[8,32,128]{2,1,0:T(8,128)S(1)}, f32[8,32,128]{2,1,0:T(8,128)S(1)}, u32[]{:S(2)}, u32[]{:S(2)}) collective-permute-start(f32[8,32,128]{2,1,0:T(8,128)S(1)} %get-tuple-element.118), channel_id=1, source_target_pairs={{0,4},{8,12},{4,0},{12,8},{1,5},{9,13},{5,1},{13,9},{2,6},{10,14},... | collective-permute-start | bytes 393224 | tf_op jit(solution)/shard_map/ppermute | solution.py:119
  51.9 2.5 %collective-permute-start.22 = (f32[8,32,128]{2,1,0:T(8,128)S(1)}, f32[8,32,128]{2,1,0:T(8,128)S(1)}, u32[]{:S(2)}, u32[]{:S(2)}) collective-permute-start(f32[8,32,128]{2,1,0:T(8,128)S(1)} %get-tuple-element.119), channel_id=1, source_target_pairs={{4,8},{0,12},{8,4},{12,0},{5,9},{1,13},{9,5},{13,1},{6,10},{2,14},... | collective-permute-start | bytes 393224 | tf_op jit(solution)/shard_map/ppermute | solution.py:119
  55.1 3.8 %collective-permute-done.17.refs_1_ = f32[8,32,128]{2,1,0:T(8,128)S(1)} collective-permute-done((f32[8,32,128]{2,1,0:T(8,128)S(1)}, f32[8,32,128]{2,1,0:T(8,128)S(1)}, u32[]{:S(2)}, u32[]{:S(2)}) %collective-permute-start.17) | collective-permute-done | bytes 131104 | tf_op jit(solution)/shard_map/ppermute | solution.py:119
  61.6 3.2 %collective-permute-start.20 = (f32[8,32,128]{2,1,0:T(8,128)S(1)}, f32[8,32,128]{2,1,0:T(8,128)S(1)}, u32[]{:S(2)}, u32[]{:S(2)}) collective-permute-start(f32[8,32,128]{2,1,0:T(8,128)S(1)} %get-tuple-element.115), channel_id=1, source_target_pairs={{0,4},{8,12},{4,0},{12,8},{1,5},{9,13},{5,1},{13,9},{2,6},{10,14},... | collective-permute-start | bytes 393224 | tf_op jit(solution)/shard_map/ppermute | solution.py:119
  66.9 5.3 %collective-permute-done.20.refs_1_ = f32[8,32,128]{2,1,0:T(8,128)S(1)} collective-permute-done((f32[8,32,128]{2,1,0:T(8,128)S(1)}, f32[8,32,128]{2,1,0:T(8,128)S(1)}, u32[]{:S(2)}, u32[]{:S(2)}) %collective-permute-start.20) | collective-permute-done | bytes 131104 | tf_op jit(solution)/shard_map/ppermute | solution.py:119
  75.4 1.7 %own.5.refs_3_ = f32[32,32,128]{2,1,0:T(8,128)S(1)} custom-call(s32[1,1,44]{2,1,0:T(1,128)S(1)} %copy-done.1, s32[1,1,44]{2,1,0:T(1,128)S(1)} %copy-done.2, f32[32,32,128]{2,1,0:T(8,128)S(1)} %get-tuple-element.124.b_ref.x_ref, bf16[44,2,128,128]{3,2,1,0:T(8,128)(2,1)S(1)} %get-tuple-element.76.refs_4_.split_ref.refs_2_.refs_6_, ...), custom_call_target="tpu_custom_call", output_to_operand_aliasing={{}: (4, {})} | custom-call | tf_op jit(solution)/shard_map/own/pallas_call | solution.py:517
  80.1 4.3 %collective-permute-done.27 = f32[64,128]{1,0:T(8,128)S(1)} collective-permute-done((f32[64,128]{1,0:T(8,128)S(1)}, f32[64,128]{1,0:T(8,128)S(1)}, u32[]{:S(2)}, u32[]{:S(2)}) %collective-permute-start.27) | collective-permute-done | bytes 32800 | tf_op jit(solution)/shard_map/ppermute | solution.py:149
  85.6 3.9 %second.1 = (f32[64,64]{1,0:T(8,128)S(1)}, f32[64,64]{1,0:T(8,128)S(1)}, f32[128,192]{1,0:T(8,128)S(1)}, f32[64,64]{1,0:T(8,128)S(1)}) custom-call(f32[64,128]{1,0:T(8,128)S(1)} %add.55.gram_ref, f32[64,64]{1,0:T(8,128)S(1)} %first.1.inverse_ref), custom_call_target="tpu_custom_call" | custom-call | tf_op jit(solution)/shard_map/second/pallas_call | solution.py:592
  89.5 1.7 %blend.3 = (f32[16,64,128]{2,1,0:T(8,128)S(1)}, f32[16,64,128]{2,1,0:T(8,128)S(1)}, f32[64,64]{1,0:T(8,128)S(1)}) custom-call(s32[4]{0:T(128)S(1)} %pad_add_fusion.place_ref, f32[32,64,128]{2,1,0:T(8,128)S(1)} %get-tuple-element.117.refs_3_.x_ref, f32[32,32,128]{2,1,0:T(8,128)S(1)} %get-tuple-element.104.x_ref.a_ref, ...), custom_call_target="tpu_custom_call" | custom-call | tf_op jit(solution)/shard_map/blend/pallas_call | solution.py:436
  91.2 1.7 %blend.2 = (f32[16,64,128]{2,1,0:T(8,128)S(1)}, f32[16,64,128]{2,1,0:T(8,128)S(1)}, f32[64,64]{1,0:T(8,128)S(1)}) custom-call(s32[4]{0:T(128)S(1)} %pad_add_fusion.place_ref, f32[32,64,128]{2,1,0:T(8,128)S(1)} %get-tuple-element.117.refs_3_.x_ref, f32[32,32,128]{2,1,0:T(8,128)S(1)} %get-tuple-element.104.x_ref.a_ref, ...), custom_call_target="tpu_custom_call" | custom-call | tf_op jit(solution)/shard_map/blend/pallas_call | solution.py:436
  93.5 1.5 %collective-permute-done.30.other_ref = f32[16,32,128]{2,1,0:T(8,128)S(1)} collective-permute-done((f32[16,32,128]{2,1,0:T(8,128)S(1)}, f32[16,32,128]{2,1,0:T(8,128)S(1)}, u32[]{:S(2)}, u32[]{:S(2)}) %collective-permute-start.30) | collective-permute-done | bytes 262176 | tf_op jit(solution)/shard_map/ppermute | solution.py:598
  95.0 2.0 %third.1 = (f32[32,64,128]{2,1,0:T(8,128)S(1)}, f32[72,128]{1,0:T(8,128)S(1)}) custom-call(s32[4]{0:T(128)S(1)} %pad_add_fusion.place_ref, f32[16,32,128]{2,1,0:T(8,128)S(1)} %add.57.mine_ref, f32[16,32,128]{2,1,0:T(8,128)S(1)} %collective-permute-done.30.other_ref, f32[64,64]{1,0:T(8,128)S(1)} %get-tuple-element.136.gain_ref, ...), custom_call_target="tpu_custom_call" | custom-call | tf_op jit(solution)/shard_map/third/pallas_call | solution.py:599
  97.0 1.7 %collective-permute-start.31 = (f32[72,128]{1,0:T(8,128)S(1)}, f32[72,128]{1,0:T(8,128)S(1)}, u32[]{:S(2)}, u32[]{:S(2)}) collective-permute-start(f32[72,128]{1,0:T(8,128)S(1)} %get-tuple-element.142), channel_id=1, source_target_pairs={{0,4},{4,0},{8,12},{12,8},{1,5},{5,1},{9,13},{13,9},{2,6},{6,2},{1... | collective-permute-start | bytes 110600 | tf_op jit(solution)/shard_map/ppermute | solution.py:140
  98.7 2.3 %collective-permute-done.31 = f32[72,128]{1,0:T(8,128)S(1)} collective-permute-done((f32[72,128]{1,0:T(8,128)S(1)}, f32[72,128]{1,0:T(8,128)S(1)}, u32[]{:S(2)}, u32[]{:S(2)}) %collective-permute-start.31) | collective-permute-done | bytes 36896 | tf_op jit(solution)/shard_map/ppermute | solution.py:140
  101.7 4.2 %collective-permute-done.32 = f32[72,128]{1,0:T(8,128)S(1)} collective-permute-done((f32[72,128]{1,0:T(8,128)S(1)}, f32[72,128]{1,0:T(8,128)S(1)}, u32[]{:S(2)}, u32[]{:S(2)}) %collective-permute-start.32) | collective-permute-done | bytes 36896 | tf_op jit(solution)/shard_map/ppermute | solution.py:149
  105.9 3.7 %fourth.1 = (f32[64,64]{1,0:T(8,128)S(1)}, f32[64,64]{1,0:T(8,128)S(1)}, f32[64,128]{1,0:T(8,128)S(1)}) custom-call(f32[72,128]{1,0:T(8,128)S(1)} %add.59.gram_ref), custom_call_target="tpu_custom_call" | custom-call | tf_op jit(solution)/shard_map/fourth/pallas_call | solution.py:607
  109.6 1.9 %last.1 = (f32[32,64,128]{2,1,0:T(8,128)}, f32[4,64,64]{2,1,0:T(8,128)}) custom-call(f32[32,64,128]{2,1,0:T(8,128)S(1)} %get-tuple-element.141.w_ref, f32[16,64,128]{2,1,0:T(8,128)S(1)} %get-tuple-element.139.refs_2_.low_ref, f32[16,64,128]{2,1,0:T(8,128)S(1)} %get-tuple-element.140.refs_3_.high_ref, f32[64,128]{1,0:T(8,128)S(1)} %get-tuple-element.143.coef_ref, ...), custom_call_target="tpu_custom_call" | custom-call | tf_op jit(solution)/shard_map/last/pallas_call | solution.py:610
  (86 shorter events, 28.8 us)
Async XLA Ops:
  0.6 8.8 %collective-permute-start.2 = (s32[1,1,44]{2,1,0:T(1,128)}, s32[1,1,44]{2,1,0:T(1,128)S(1)}, u32[]{:S(2)}, u32[]{:S(2)}) collective-permute-start(s32[1,1,44]{2,1,0:T(1,128)} %cols_ref.5), channel_id=1, source_target_pairs={{4,8},{0,12},{8,4},{12,0},{5,9},{1,13},{9,5},{13,1},{6,10},{2,14},... | collective-permute-start | bytes 536 | tf_op jit(solution)/shard_map/ppermute | solution.py:119
  5.8 3.7 %collective-permute-start.1 = (s32[1,1,44]{2,1,0:T(1,128)}, s32[1,1,44]{2,1,0:T(1,128)S(1)}, u32[]{:S(2)}, u32[]{:S(2)}) collective-permute-start(s32[1,1,44]{2,1,0:T(1,128)} %cols_ref.5), channel_id=1, source_target_pairs={{0,4},{8,12},{4,0},{12,8},{1,5},{9,13},{5,1},{13,9},{2,6},{10,14},... | collective-permute-start | bytes 536 | tf_op jit(solution)/shard_map/ppermute | solution.py:119
  5.8 4.6 %collective-permute-start = (s32[1,1,44]{2,1,0:T(1,128)}, s32[1,1,44]{2,1,0:T(1,128)S(1)}, u32[]{:S(2)}, u32[]{:S(2)}) collective-permute-start(s32[1,1,44]{2,1,0:T(1,128)} %cols_ref.5), channel_id=1, source_target_pairs={{0,8},{4,12},{8,0},{12,4},{1,9},{5,13},{9,1},{13,5},{2,10},{6,14},... | collective-permute-start | bytes 536 | tf_op jit(solution)/shard_map/ppermute | solution.py:119
  11.8 6.5 %collective-permute-start.5 = (f32[8,32,128]{2,1,0:T(8,128)S(1)}, f32[8,32,128]{2,1,0:T(8,128)S(1)}, u32[]{:S(2)}, u32[]{:S(2)}) collective-permute-start(f32[8,32,128]{2,1,0:T(8,128)S(1)} %get-tuple-element.80), channel_id=1, source_target_pairs={{0,4},{8,12},{4,0},{12,8},{1,5},{9,13},{5,1},{13,9},{2,6},{10,14},... | collective-permute-start | bytes 393224 | tf_op jit(solution)/shard_map/ppermute | solution.py:119
  13.6 14.3 %collective-permute-start.3 = (f32[8,32,128]{2,1,0:T(8,128)S(1)}, f32[8,32,128]{2,1,0:T(8,128)S(1)}, u32[]{:S(2)}, u32[]{:S(2)}) collective-permute-start(f32[8,32,128]{2,1,0:T(8,128)S(1)} %get-tuple-element.78), channel_id=1, source_target_pairs={{0,8},{4,12},{8,0},{12,4},{1,9},{5,13},{9,1},{13,5},{2,10},{6,14},... | collective-permute-start | bytes 393224 | tf_op jit(solution)/shard_map/ppermute | solution.py:119
  14.6 8.3 %collective-permute-start.4 = (f32[8,32,128]{2,1,0:T(8,128)S(1)}, f32[8,32,128]{2,1,0:T(8,128)S(1)}, u32[]{:S(2)}, u32[]{:S(2)}) collective-permute-start(f32[8,32,128]{2,1,0:T(8,128)S(1)} %get-tuple-element.79), channel_id=1, source_target_pairs={{4,8},{0,12},{8,4},{12,0},{5,9},{1,13},{9,5},{13,1},{6,10},{2,14},... | collective-permute-start | bytes 393224 | tf_op jit(solution)/shard_map/ppermute | solution.py:119
  19.8 8.0 %collective-permute-start.6 = (f32[64,64]{1,0:T(8,128)S(1)}, f32[64,64]{1,0:T(8,128)S(1)}, u32[]{:S(2)}, u32[]{:S(2)}) collective-permute-start(f32[64,64]{1,0:T(8,128)S(1)} %gram.1), channel_id=1, source_target_pairs={{0,4},{4,0},{8,12},{12,8},{1,5},{5,1},{9,13},{13,9},{2,6},{6,2},{1... | collective-permute-start | bytes 49160 | tf_op jit(solution)/shard_map/ppermute | solution.py:140
  23.9 9.5 %collective-permute-start.9 = (f32[8,32,128]{2,1,0:T(8,128)S(1)}, f32[8,32,128]{2,1,0:T(8,128)S(1)}, u32[]{:S(2)}, u32[]{:S(2)}) collective-permute-start(f32[8,32,128]{2,1,0:T(8,128)S(1)} %get-tuple-element.94), channel_id=1, source_target_pairs={{0,4},{8,12},{4,0},{12,8},{1,5},{9,13},{5,1},{13,9},{2,6},{10,14},... | collective-permute-start | bytes 393224 | tf_op jit(solution)/shard_map/ppermute | solution.py:119
  27.8 11.2 %collective-permute-start.10 = (f32[64,64]{1,0:T(8,128)S(1)}, f32[64,64]{1,0:T(8,128)S(1)}, u32[]{:S(2)}, u32[]{:S(2)}) collective-permute-start(f32[64,64]{1,0:T(8,128)S(1)} %add.46), channel_id=1, source_target_pairs={{0,8},{4,12},{8,0},{12,4},{1,9},{5,13},{9,1},{13,5},{2,10},{6,14},... | collective-permute-start | bytes 49160 | tf_op jit(solution)/shard_map/ppermute | solution.py:149
  29.0 14.5 %collective-permute-start.7 = (f32[8,32,128]{2,1,0:T(8,128)S(1)}, f32[8,32,128]{2,1,0:T(8,128)S(1)}, u32[]{:S(2)}, u32[]{:S(2)}) collective-permute-start(f32[8,32,128]{2,1,0:T(8,128)S(1)} %get-tuple-element.91), channel_id=1, source_target_pairs={{0,8},{4,12},{8,0},{12,4},{1,9},{5,13},{9,1},{13,5},{2,10},{6,14},... | collective-permute-start | bytes 393224 | tf_op jit(solution)/shard_map/ppermute | solution.py:119
  31.6 10.4 %collective-permute-start.8 = (f32[8,32,128]{2,1,0:T(8,128)S(1)}, f32[8,32,128]{2,1,0:T(8,128)S(1)}, u32[]{:S(2)}, u32[]{:S(2)}) collective-permute-start(f32[8,32,128]{2,1,0:T(8,128)S(1)} %get-tuple-element.93), channel_id=1, source_target_pairs={{4,8},{0,12},{8,4},{12,0},{5,9},{1,13},{9,5},{13,1},{6,10},{2,14},... | collective-permute-start | bytes 393224 | tf_op jit(solution)/shard_map/ppermute | solution.py:119
  35.0 8.4 %collective-permute-start.13 = (f32[16,32,128]{2,1,0:T(8,128)S(1)}, f32[16,32,128]{2,1,0:T(8,128)S(1)}, u32[]{:S(2)}, u32[]{:S(2)}) collective-permute-start(f32[16,32,128]{2,1,0:T(8,128)S(1)} %add.47), channel_id=1, source_target_pairs={{0,2},{1,3},{2,0},{3,1},{4,6},{5,7},{6,4},{7,5},{8,10},{9,11},{10,... | collective-permute-start | bytes 786440 | tf_op jit(solution)/shard_map/ppermute | solution.py:502
  43.4 1.7 %collective-permute-start.14 = (f32[16,32,128]{2,1,0:T(8,128)S(1)}, f32[16,32,128]{2,1,0:T(8,128)S(1)}, u32[]{:S(2)}, u32[]{:S(2)}) collective-permute-start(f32[16,32,128]{2,1,0:T(8,128)S(1)} %add.49.refs_3_), channel_id=1, source_target_pairs={{0,1},{1,0},{2,3},{3,2},{4,5},{5,4},{6,7},{7,6},{8,9},{9,8},{10,11... | collective-permute-start | bytes 786440 | tf_op jit(solution)/shard_map/ppermute | solution.py:564
  44.6 2.0 %collective-permute-start.12 = (f32[16,32,128]{2,1,0:T(8,128)S(1)}, f32[16,32,128]{2,1,0:T(8,128)S(1)}, u32[]{:S(2)}, u32[]{:S(2)}) collective-permute-start(f32[16,32,128]{2,1,0:T(8,128)S(1)} %get-tuple-element.101), channel_id=1, source_target_pairs={{0,1},{1,0},{2,3},{3,2},{4,5},{5,4},{6,7},{7,6},{8,9},{9,8},{10,11... | collective-permute-start | bytes 786440 | tf_op jit(solution)/shard_map/ppermute | solution.py:568
  46.6 8.3 %collective-permute-start.15 = (f32[16,32,128]{2,1,0:T(8,128)S(1)}, f32[16,32,128]{2,1,0:T(8,128)S(1)}, u32[]{:S(2)}, u32[]{:S(2)}) collective-permute-start(f32[16,32,128]{2,1,0:T(8,128)S(1)} %add.50), channel_id=1, source_target_pairs={{0,2},{1,3},{2,0},{3,1},{4,6},{5,7},{6,4},{7,5},{8,10},{9,11},{10,... | collective-permute-start | bytes 786440 | tf_op jit(solution)/shard_map/ppermute | solution.py:502
  48.2 10.7 %collective-permute-start.17 = (f32[8,32,128]{2,1,0:T(8,128)S(1)}, f32[8,32,128]{2,1,0:T(8,128)S(1)}, u32[]{:S(2)}, u32[]{:S(2)}) collective-permute-start(f32[8,32,128]{2,1,0:T(8,128)S(1)} %get-tuple-element.109), channel_id=1, source_target_pairs={{0,8},{4,12},{8,0},{12,4},{1,9},{5,13},{9,1},{13,5},{2,10},{6,14},... | collective-permute-start | bytes 393224 | tf_op jit(solution)/shard_map/ppermute | solution.py:119
  50.4 15.4 %collective-permute-start.21 = (f32[8,32,128]{2,1,0:T(8,128)S(1)}, f32[8,32,128]{2,1,0:T(8,128)S(1)}, u32[]{:S(2)}, u32[]{:S(2)}) collective-permute-start(f32[8,32,128]{2,1,0:T(8,128)S(1)} %get-tuple-element.118), channel_id=1, source_target_pairs={{0,4},{8,12},{4,0},{12,8},{1,5},{9,13},{5,1},{13,9},{2,6},{10,14},... | collective-permute-start | bytes 393224 | tf_op jit(solution)/shard_map/ppermute | solution.py:119
  51.9 12.9 %collective-permute-start.22 = (f32[8,32,128]{2,1,0:T(8,128)S(1)}, f32[8,32,128]{2,1,0:T(8,128)S(1)}, u32[]{:S(2)}, u32[]{:S(2)}) collective-permute-start(f32[8,32,128]{2,1,0:T(8,128)S(1)} %get-tuple-element.119), channel_id=1, source_target_pairs={{4,8},{0,12},{8,4},{12,0},{5,9},{1,13},{9,5},{13,1},{6,10},{2,14},... | collective-permute-start | bytes 393224 | tf_op jit(solution)/shard_map/ppermute | solution.py:119
  55.0 4.8 %collective-permute-start.16 = (f32[16,32,128]{2,1,0:T(8,128)S(1)}, f32[16,32,128]{2,1,0:T(8,128)S(1)}, u32[]{:S(2)}, u32[]{:S(2)}) collective-permute-start(f32[16,32,128]{2,1,0:T(8,128)S(1)} %add.51.refs_3_), channel_id=1, source_target_pairs={{0,1},{1,0},{2,3},{3,2},{4,5},{5,4},{6,7},{7,6},{8,9},{9,8},{10,11... | collective-permute-start | bytes 786440 | tf_op jit(solution)/shard_map/ppermute | solution.py:572
  61.3 17.1 %collective-permute-start.18 = (f32[8,32,128]{2,1,0:T(8,128)S(1)}, f32[8,32,128]{2,1,0:T(8,128)S(1)}, u32[]{:S(2)}, u32[]{:S(2)}) collective-permute-start(f32[8,32,128]{2,1,0:T(8,128)S(1)} %get-tuple-element.112), channel_id=1, source_target_pairs={{0,8},{4,12},{8,0},{12,4},{1,9},{5,13},{9,1},{13,5},{2,10},{6,14},... | collective-permute-start | bytes 393224 | tf_op jit(solution)/shard_map/ppermute | solution.py:119
  61.4 15.8 %collective-permute-start.19 = (f32[8,32,128]{2,1,0:T(8,128)S(1)}, f32[8,32,128]{2,1,0:T(8,128)S(1)}, u32[]{:S(2)}, u32[]{:S(2)}) collective-permute-start(f32[8,32,128]{2,1,0:T(8,128)S(1)} %get-tuple-element.113), channel_id=1, source_target_pairs={{4,8},{0,12},{8,4},{12,0},{5,9},{1,13},{9,5},{13,1},{6,10},{2,14},... | collective-permute-start | bytes 393224 | tf_op jit(solution)/shard_map/ppermute | solution.py:119
  61.6 10.6 %collective-permute-start.20 = (f32[8,32,128]{2,1,0:T(8,128)S(1)}, f32[8,32,128]{2,1,0:T(8,128)S(1)}, u32[]{:S(2)}, u32[]{:S(2)}) collective-permute-start(f32[8,32,128]{2,1,0:T(8,128)S(1)} %get-tuple-element.115), channel_id=1, source_target_pairs={{0,4},{8,12},{4,0},{12,8},{1,5},{9,13},{5,1},{13,9},{2,6},{10,14},... | collective-permute-start | bytes 393224 | tf_op jit(solution)/shard_map/ppermute | solution.py:119
  66.8 6.5 %collective-permute-start.23 = (f32[16,32,128]{2,1,0:T(8,128)S(1)}, f32[16,32,128]{2,1,0:T(8,128)S(1)}, u32[]{:S(2)}, u32[]{:S(2)}) collective-permute-start(f32[16,32,128]{2,1,0:T(8,128)S(1)} %get-tuple-element.122), channel_id=1, source_target_pairs={{0,1},{1,0},{2,3},{3,2},{4,5},{5,4},{6,7},{7,6},{8,9},{9,8},{10,11... | collective-permute-start | bytes 786440 | tf_op jit(solution)/shard_map/ppermute | solution.py:578
  74.4 4.0 %collective-permute-start.24 = (f32[64,128]{1,0:T(8,128)S(1)}, f32[64,128]{1,0:T(8,128)S(1)}, u32[]{:S(2)}, u32[]{:S(2)}) collective-permute-start(f32[64,128]{1,0:T(8,128)S(1)} %cross.1), channel_id=1, source_target_pairs={{0,4},{4,0},{8,12},{12,8},{1,5},{5,1},{9,13},{13,9},{2,6},{6,2},{1... | collective-permute-start | bytes 98312 | tf_op jit(solution)/shard_map/ppermute | solution.py:140
  74.5 9.9 %collective-permute-start.26 = (f32[16,32,128]{2,1,0:T(8,128)S(1)}, f32[16,32,128]{2,1,0:T(8,128)S(1)}, u32[]{:S(2)}, u32[]{:S(2)}) collective-permute-start(f32[16,32,128]{2,1,0:T(8,128)S(1)} %add.52), channel_id=1, source_target_pairs={{0,2},{1,3},{2,0},{3,1},{4,6},{5,7},{6,4},{7,5},{8,10},{9,11},{10,... | collective-permute-start | bytes 786440 | tf_op jit(solution)/shard_map/ppermute | solution.py:502
  79.4 5.1 %collective-permute-start.25 = (f32[16,32,128]{2,1,0:T(8,128)S(1)}, f32[16,32,128]{2,1,0:T(8,128)S(1)}, u32[]{:S(2)}, u32[]{:S(2)}) collective-permute-start(f32[16,32,128]{2,1,0:T(8,128)S(1)} %get-tuple-element.128), channel_id=1, source_target_pairs={{0,1},{1,0},{2,3},{3,2},{4,5},{5,4},{6,7},{7,6},{8,9},{9,8},{10,11... | collective-permute-start | bytes 786440 | tf_op jit(solution)/shard_map/ppermute | solution.py:587
  79.5 4.9 %collective-permute-start.27 = (f32[64,128]{1,0:T(8,128)S(1)}, f32[64,128]{1,0:T(8,128)S(1)}, u32[]{:S(2)}, u32[]{:S(2)}) collective-permute-start(f32[64,128]{1,0:T(8,128)S(1)} %add.53), channel_id=1, source_target_pairs={{0,8},{4,12},{8,0},{12,4},{1,9},{5,13},{9,1},{13,5},{2,10},{6,14},... | collective-permute-start | bytes 98312 | tf_op jit(solution)/shard_map/ppermute | solution.py:149
  84.4 5.1 %collective-permute-start.29 = (f32[16,32,128]{2,1,0:T(8,128)S(1)}, f32[16,32,128]{2,1,0:T(8,128)S(1)}, u32[]{:S(2)}, u32[]{:S(2)}) collective-permute-start(f32[16,32,128]{2,1,0:T(8,128)S(1)} %add.54.mine_ref), channel_id=1, source_target_pairs={{0,1},{1,0},{2,3},{3,2},{4,5},{5,4},{6,7},{7,6},{8,9},{9,8},{10,11... | collective-permute-start | bytes 786440 | tf_op jit(solution)/shard_map/ppermute | solution.py:589
  84.6 8.8 %collective-permute-start.28 = (f32[16,32,128]{2,1,0:T(8,128)S(1)}, f32[16,32,128]{2,1,0:T(8,128)S(1)}, u32[]{:S(2)}, u32[]{:S(2)}) collective-permute-start(f32[16,32,128]{2,1,0:T(8,128)S(1)} %add.56), channel_id=1, source_target_pairs={{0,2},{1,3},{2,0},{3,1},{4,6},{5,7},{6,4},{7,5},{8,10},{9,11},{10,... | collective-permute-start | bytes 786440 | tf_op jit(solution)/shard_map/ppermute | solution.py:502
  93.4 1.6 %collective-permute-start.30 = (f32[16,32,128]{2,1,0:T(8,128)S(1)}, f32[16,32,128]{2,1,0:T(8,128)S(1)}, u32[]{:S(2)}, u32[]{:S(2)}) collective-permute-start(f32[16,32,128]{2,1,0:T(8,128)S(1)} %add.57.mine_ref), channel_id=1, source_target_pairs={{0,1},{1,0},{2,3},{3,2},{4,5},{5,4},{6,7},{7,6},{8,9},{9,8},{10,11... | collective-permute-start | bytes 786440 | tf_op jit(solution)/shard_map/ppermute | solution.py:598
  97.0 4.0 %collective-permute-start.31 = (f32[72,128]{1,0:T(8,128)S(1)}, f32[72,128]{1,0:T(8,128)S(1)}, u32[]{:S(2)}, u32[]{:S(2)}) collective-permute-start(f32[72,128]{1,0:T(8,128)S(1)} %get-tuple-element.142), channel_id=1, source_target_pairs={{0,4},{4,0},{8,12},{12,8},{1,5},{5,1},{9,13},{13,9},{2,6},{6,2},{1... | collective-permute-start | bytes 110600 | tf_op jit(solution)/shard_map/ppermute | solution.py:140
  101.0 4.9 %collective-permute-start.32 = (f32[72,128]{1,0:T(8,128)S(1)}, f32[72,128]{1,0:T(8,128)S(1)}, u32[]{:S(2)}, u32[]{:S(2)}) collective-permute-start(f32[72,128]{1,0:T(8,128)S(1)} %add.58), channel_id=1, source_target_pairs={{0,8},{4,12},{8,0},{12,4},{1,9},{5,13},{9,1},{13,5},{2,10},{6,14},... | collective-permute-start | bytes 110600 | tf_op jit(solution)/shard_map/ppermute | solution.py:149
  (5 other events, 29.4 us)

commit v12 on v11

--- a/solution.py
+++ b/solution.py
@@ -576,19 +576,19 @@
     keep_a, give_a = join(acc_a, got_a, groups[0], last=True)
 
     core = lax.ppermute(give_a, "vec", swap)
+    (gram,) = call(cross_body, [(width, 2 * width)], [VMEM] * 3, name="cross")(x, y_a, after(y_b, keep_a))
+    (acc_b,) = own(y_b, after(acc_b, gram))
+    cross_gram = start_sum(gram, "res")
     acc_b = join(acc_b, got_b, groups[0])
     mine_a = keep_a + after(core, acc_b)
-    (gram,) = call(cross_body, [(width, 2 * width)], [VMEM] * 3, name="cross")(x, y_a, after(y_b, mine_a))
-    (acc_b,) = own(y_b, after(acc_b, gram))
-    acc_b = join(acc_b, got_b, groups[1])
-    cross_gram = start_sum(gram, "res")
+    acc_b = join(after(acc_b, mine_a, cross_gram), got_b, groups[1])
+    cross_gram = end_sum(cross_gram, "res", acc_b)
     keep_b, give_b = join(after(acc_b, cross_gram), got_b, groups[2], last=True)
 
+    mine_a = across(mine_a, keep_b)
+    other_a = lax.ppermute(mine_a, "vec", swap)
     core = lax.ppermute(give_b, "vec", swap)
-    mine_a = across(mine_a, cross_gram)
-    other_a = lax.ppermute(mine_a, "vec", swap)
-    cross_gram = end_sum(cross_gram, "res")
-    mine_b = keep_b + after(core, mine_a, cross_gram)
+    mine_b = keep_b + after(core, mine_a)
     cross1, lower1, coef, gain = call(
         second_body, [square, square, (2 * width, 3 * width), square], [VMEM] * 2, name="second"
     )(after(cross_gram, mine_b), start_inv)

time: 112 us -> 112 us (level)
    ppermute x15, waiting for transfers between devices: 11.6 us -> 9.93 us  [exchange(): lax.ppermute(block, axis, [(a, b) for a, b in pairs] + [(b, a) for a, b i...]
    ppermute x3, starting transfers between devices: 3.26 us -> 4.44 us  [start_sum(): lax.ppermute(block, axis, [(i, i ^ step) for i in range(size)])]
where the time goes in v12:
time: 112 us
  Pallas kernels  43.4 us (39%)
  starting transfers between devices  38.1 us (34%)
  waiting for transfers between devices  28.2 us (25%)
    ppermute x15, starting transfers between devices, exchange(): lax.ppermute(block, axis, [(a, b) for a, b in pairs] + [(b, a) for a, b i...  25.9 us
    pallas_call x12, Pallas kernels, join(): call(body, [halfchunk] * 2 if last else [chunk], [SMEM] * (3 + size) + [V...  11.9 us
    ppermute x3, waiting for transfers between devices, end_sum(): got = lax.ppermute(block, axis, [(i, i ^ step) for i in range(size)])  11.1 us
    ppermute x15, waiting for transfers between devices, exchange(): lax.ppermute(block, axis, [(a, b) for a, b in pairs] + [(b, a) for a, b i...  9.93 us
    pallas_call x3, Pallas kernels, own(): call(own_body, [chunk] * len(accs), [SMEM] * 2 + [VMEM] * (2 + len(accs))...  5.46 us
    ppermute x3, starting transfers between devices, start_sum(): lax.ppermute(block, axis, [(i, i ^ step) for i in range(size)])  4.44 us
    ppermute x4, starting transfers between devices, across(): got = lax.ppermute(mine, 'vec', [(i, i ^ step) for i in range(lanes)])  4.31 us
    pallas_call x1, Pallas kernels, local(): call(second_body, [square, square, (2 * width, 3 * width), square], [VMEM...  3.94 us
  transfers between devices with their start and end apart: 33, of which 14 were waited for; matrix products, arithmetic and copies ran while one was open for 1% of the time, Pallas kernels for 31%

profile of v12, /device:TPU:0, one launch (start us, length us, event | category | flops | bytes accessed | tf_op | source)
XLA Modules:
  0.0 112.0 jit_solution(2556195591442344688)
XLA Ops:
  0.6 5.1 %collective-permute-start.2 = (s32[1,1,44]{2,1,0:T(1,128)}, s32[1,1,44]{2,1,0:T(1,128)S(1)}, u32[]{:S(2)}, u32[]{:S(2)}) collective-permute-start(s32[1,1,44]{2,1,0:T(1,128)} %cols_ref.5), channel_id=1, source_target_pairs={{4,8},{0,12},{8,4},{12,0},{5,9},{1,13},{9,5},{13,1},{6,10},{2,14},... | collective-permute-start | bytes 536 | tf_op jit(solution)/shard_map/ppermute | solution.py:119
  7.2 2.3 %prepare.1 = (f32[32,64,128]{2,1,0:T(8,128)S(1)}, bf16[44,2,128,128]{3,2,1,0:T(8,128)(2,1)S(1)}, f32[32,32,128]{2,1,0:T(8,128)S(1)}, f32[32,32,128]{2,1,0:T(8,128)S(1)}) custom-call(f32[32,64,128]{2,1,0:T(8,128)} %x_hbm.1, f32[32,128]{1,0:T(8,128)} %refs_5_.3, f32[1,1,44,128,128]{4,3,2,1,0:T(8,128)} %tiles_hbm.1), custom_call_target="tpu_custom_call" | custom-call | tf_op jit(solution)/shard_map/prepare/pallas_call | solution.py:526
  11.8 1.8 %collective-permute-start.5 = (f32[8,32,128]{2,1,0:T(8,128)S(1)}, f32[8,32,128]{2,1,0:T(8,128)S(1)}, u32[]{:S(2)}, u32[]{:S(2)}) collective-permute-start(f32[8,32,128]{2,1,0:T(8,128)S(1)} %get-tuple-element.82), channel_id=1, source_target_pairs={{0,4},{8,12},{4,0},{12,8},{1,5},{9,13},{5,1},{13,9},{2,6},{10,14},... | collective-permute-start | bytes 393224 | tf_op jit(solution)/shard_map/ppermute | solution.py:119
  14.6 1.6 %collective-permute-start.4 = (f32[8,32,128]{2,1,0:T(8,128)S(1)}, f32[8,32,128]{2,1,0:T(8,128)S(1)}, u32[]{:S(2)}, u32[]{:S(2)}) collective-permute-start(f32[8,32,128]{2,1,0:T(8,128)S(1)} %get-tuple-element.81), channel_id=1, source_target_pairs={{4,8},{0,12},{8,4},{12,0},{5,9},{1,13},{9,5},{13,1},{6,10},{2,14},... | collective-permute-start | bytes 393224 | tf_op jit(solution)/shard_map/ppermute | solution.py:119
  16.2 2.0 %own.3 = (f32[32,32,128]{2,1,0:T(8,128)S(1)}, f32[32,32,128]{2,1,0:T(8,128)S(1)}) custom-call(s32[1,1,44]{2,1,0:T(1,128)S(1)} %copy-done.1, s32[1,1,44]{2,1,0:T(1,128)S(1)} %copy-done.2, f32[32,64,128]{2,1,0:T(8,128)S(1)} %get-tuple-element.119.refs_3_.x_ref, ...), custom_call_target="tpu_custom_call", output_to_operand_aliasing={{0}: (4, {}), {1}: (5, {})} | custom-call | tf_op jit(solution)/shard_map/own/pallas_call | solution.py:517
  19.8 1.5 %collective-permute-start.6 = (f32[64,64]{1,0:T(8,128)S(1)}, f32[64,64]{1,0:T(8,128)S(1)}, u32[]{:S(2)}, u32[]{:S(2)}) collective-permute-start(f32[64,64]{1,0:T(8,128)S(1)} %gram.1), channel_id=1, source_target_pairs={{0,4},{4,0},{8,12},{12,8},{1,5},{5,1},{9,13},{13,9},{2,6},{6,2},{1... | collective-permute-start | bytes 49160 | tf_op jit(solution)/shard_map/ppermute | solution.py:140
  21.2 1.7 %collective-permute-done.4.refs_1_ = f32[8,32,128]{2,1,0:T(8,128)S(1)} collective-permute-done((f32[8,32,128]{2,1,0:T(8,128)S(1)}, f32[8,32,128]{2,1,0:T(8,128)S(1)}, u32[]{:S(2)}, u32[]{:S(2)}) %collective-permute-start.4) | collective-permute-done | bytes 131104 | tf_op jit(solution)/shard_map/ppermute | solution.py:119
  23.9 3.9 %collective-permute-start.9 = (f32[8,32,128]{2,1,0:T(8,128)S(1)}, f32[8,32,128]{2,1,0:T(8,128)S(1)}, u32[]{:S(2)}, u32[]{:S(2)}) collective-permute-start(f32[8,32,128]{2,1,0:T(8,128)S(1)} %get-tuple-element.96), channel_id=1, source_target_pairs={{0,4},{8,12},{4,0},{12,8},{1,5},{9,13},{5,1},{13,9},{2,6},{10,14},... | collective-permute-start | bytes 393224 | tf_op jit(solution)/shard_map/ppermute | solution.py:119
  29.0 2.6 %collective-permute-start.7 = (f32[8,32,128]{2,1,0:T(8,128)S(1)}, f32[8,32,128]{2,1,0:T(8,128)S(1)}, u32[]{:S(2)}, u32[]{:S(2)}) collective-permute-start(f32[8,32,128]{2,1,0:T(8,128)S(1)} %get-tuple-element.93), channel_id=1, source_target_pairs={{0,8},{4,12},{8,0},{12,4},{1,9},{5,13},{9,1},{13,5},{2,10},{6,14},... | collective-permute-start | bytes 393224 | tf_op jit(solution)/shard_map/ppermute | solution.py:119
  31.6 1.9 %collective-permute-start.8 = (f32[8,32,128]{2,1,0:T(8,128)S(1)}, f32[8,32,128]{2,1,0:T(8,128)S(1)}, u32[]{:S(2)}, u32[]{:S(2)}) collective-permute-start(f32[8,32,128]{2,1,0:T(8,128)S(1)} %get-tuple-element.95), channel_id=1, source_target_pairs={{4,8},{0,12},{8,4},{12,0},{5,9},{1,13},{9,5},{13,1},{6,10},{2,14},... | collective-permute-start | bytes 393224 | tf_op jit(solution)/shard_map/ppermute | solution.py:119
  35.0 1.6 %collective-permute-start.13 = (f32[16,32,128]{2,1,0:T(8,128)S(1)}, f32[16,32,128]{2,1,0:T(8,128)S(1)}, u32[]{:S(2)}, u32[]{:S(2)}) collective-permute-start(f32[16,32,128]{2,1,0:T(8,128)S(1)} %add.47), channel_id=1, source_target_pairs={{0,2},{1,3},{2,0},{3,1},{4,6},{5,7},{6,4},{7,5},{8,10},{9,11},{10,... | collective-permute-start | bytes 786440 | tf_op jit(solution)/shard_map/ppermute | solution.py:502
  36.5 2.5 %collective-permute-done.10 = f32[64,64]{1,0:T(8,128)S(1)} collective-permute-done((f32[64,64]{1,0:T(8,128)S(1)}, f32[64,64]{1,0:T(8,128)S(1)}, u32[]{:S(2)}, u32[]{:S(2)}) %collective-permute-start.10) | collective-permute-done | bytes 16416 | tf_op jit(solution)/shard_map/ppermute | solution.py:149
  39.0 3.0 %first.1.inverse_ref = f32[64,64]{1,0:T(8,128)S(1)} custom-call(f32[64,64]{1,0:T(8,128)S(1)} %add.48.gram_ref), custom_call_target="tpu_custom_call" | custom-call | tf_op jit(solution)/shard_map/first/pallas_call | solution.py:561
  46.6 1.6 %collective-permute-start.15 = (f32[16,32,128]{2,1,0:T(8,128)S(1)}, f32[16,32,128]{2,1,0:T(8,128)S(1)}, u32[]{:S(2)}, u32[]{:S(2)}) collective-permute-start(f32[16,32,128]{2,1,0:T(8,128)S(1)} %add.50), channel_id=1, source_target_pairs={{0,2},{1,3},{2,0},{3,1},{4,6},{5,7},{6,4},{7,5},{8,10},{9,11},{10,... | collective-permute-start | bytes 786440 | tf_op jit(solution)/shard_map/ppermute | solution.py:502
  48.6 1.7 %own.4.refs_3_ = f32[32,32,128]{2,1,0:T(8,128)S(1)} custom-call(s32[1,1,44]{2,1,0:T(1,128)S(1)} %copy-done.1, s32[1,1,44]{2,1,0:T(1,128)S(1)} %copy-done.2, f32[32,32,128]{2,1,0:T(8,128)S(1)} %get-tuple-element.106.x_ref.a_ref, bf16[44,2,128,128]{3,2,1,0:T(8,128)(2,1)S(1)} %get-tuple-element.78.refs_4_.split_ref.refs_2_.refs_6_, ...), custom_call_target="tpu_custom_call", output_to_operand_aliasing={{}: (4, {})} | custom-call | tf_op jit(solution)/shard_map/own/pallas_call | solution.py:517
  50.4 1.5 %collective-permute-start.21 = (f32[8,32,128]{2,1,0:T(8,128)S(1)}, f32[8,32,128]{2,1,0:T(8,128)S(1)}, u32[]{:S(2)}, u32[]{:S(2)}) collective-permute-start(f32[8,32,128]{2,1,0:T(8,128)S(1)} %get-tuple-element.120), channel_id=1, source_target_pairs={{0,4},{8,12},{4,0},{12,8},{1,5},{9,13},{5,1},{13,9},{2,6},{10,14},... | collective-permute-start | bytes 393224 | tf_op jit(solution)/shard_map/ppermute | solution.py:119
  51.9 2.5 %collective-permute-start.22 = (f32[8,32,128]{2,1,0:T(8,128)S(1)}, f32[8,32,128]{2,1,0:T(8,128)S(1)}, u32[]{:S(2)}, u32[]{:S(2)}) collective-permute-start(f32[8,32,128]{2,1,0:T(8,128)S(1)} %get-tuple-element.121), channel_id=1, source_target_pairs={{4,8},{0,12},{8,4},{12,0},{5,9},{1,13},{9,5},{13,1},{6,10},{2,14},... | collective-permute-start | bytes 393224 | tf_op jit(solution)/shard_map/ppermute | solution.py:119
  55.1 3.8 %collective-permute-done.17.refs_1_ = f32[8,32,128]{2,1,0:T(8,128)S(1)} collective-permute-done((f32[8,32,128]{2,1,0:T(8,128)S(1)}, f32[8,32,128]{2,1,0:T(8,128)S(1)}, u32[]{:S(2)}, u32[]{:S(2)}) %collective-permute-start.17) | collective-permute-done | bytes 131104 | tf_op jit(solution)/shard_map/ppermute | solution.py:119
  64.6 1.7 %collective-permute-start.24 = (f32[64,128]{1,0:T(8,128)S(1)}, f32[64,128]{1,0:T(8,128)S(1)}, u32[]{:S(2)}, u32[]{:S(2)}) collective-permute-start(f32[64,128]{1,0:T(8,128)S(1)} %cross.1), channel_id=1, source_target_pairs={{0,4},{4,0},{8,12},{12,8},{1,5},{5,1},{9,13},{13,9},{2,6},{6,2},{1... | collective-permute-start | bytes 98312 | tf_op jit(solution)/shard_map/ppermute | solution.py:140
  66.3 1.7 %own.5.refs_3_ = f32[32,32,128]{2,1,0:T(8,128)S(1)} custom-call(s32[1,1,44]{2,1,0:T(1,128)S(1)} %copy-done.1, s32[1,1,44]{2,1,0:T(1,128)S(1)} %copy-done.2, f32[32,32,128]{2,1,0:T(8,128)S(1)} %get-tuple-element.124.b_ref.x_ref, bf16[44,2,128,128]{3,2,1,0:T(8,128)(2,1)S(1)} %get-tuple-element.78.refs_4_.split_ref.refs_2_.refs_6_, ...), custom_call_target="tpu_custom_call", output_to_operand_aliasing={{}: (4, {})} | custom-call | tf_op jit(solution)/shard_map/own/pallas_call | solution.py:517
  68.7 2.1 %collective-permute-start.19 = (f32[8,32,128]{2,1,0:T(8,128)S(1)}, f32[8,32,128]{2,1,0:T(8,128)S(1)}, u32[]{:S(2)}, u32[]{:S(2)}) collective-permute-start(f32[8,32,128]{2,1,0:T(8,128)S(1)} %get-tuple-element.115), channel_id=1, source_target_pairs={{4,8},{0,12},{8,4},{12,0},{5,9},{1,13},{9,5},{13,1},{6,10},{2,14},... | collective-permute-start | bytes 393224 | tf_op jit(solution)/shard_map/ppermute | solution.py:119
  73.3 3.6 %collective-permute-done.19.refs_1_ = f32[8,32,128]{2,1,0:T(8,128)S(1)} collective-permute-done((f32[8,32,128]{2,1,0:T(8,128)S(1)}, f32[8,32,128]{2,1,0:T(8,128)S(1)}, u32[]{:S(2)}, u32[]{:S(2)}) %collective-permute-start.19) | collective-permute-done | bytes 131104 | tf_op jit(solution)/shard_map/ppermute | solution.py:119
  77.9 4.9 %collective-permute-done.25 = f32[64,128]{1,0:T(8,128)S(1)} collective-permute-done((f32[64,128]{1,0:T(8,128)S(1)}, f32[64,128]{1,0:T(8,128)S(1)}, u32[]{:S(2)}, u32[]{:S(2)}) %collective-permute-start.25) | collective-permute-done | bytes 32800 | tf_op jit(solution)/shard_map/ppermute | solution.py:149
  86.1 3.9 %second.1 = (f32[64,64]{1,0:T(8,128)S(1)}, f32[64,64]{1,0:T(8,128)S(1)}, f32[128,192]{1,0:T(8,128)S(1)}, f32[64,64]{1,0:T(8,128)S(1)}) custom-call(f32[64,128]{1,0:T(8,128)S(1)} %add.54.gram_ref, f32[64,64]{1,0:T(8,128)S(1)} %first.1.inverse_ref), custom_call_target="tpu_custom_call" | custom-call | tf_op jit(solution)/shard_map/second/pallas_call | solution.py:592
  90.0 1.7 %blend.3 = (f32[16,64,128]{2,1,0:T(8,128)S(1)}, f32[16,64,128]{2,1,0:T(8,128)S(1)}, f32[64,64]{1,0:T(8,128)S(1)}) custom-call(s32[4]{0:T(128)S(1)} %pad_add_fusion.place_ref, f32[32,64,128]{2,1,0:T(8,128)S(1)} %get-tuple-element.119.refs_3_.x_ref, f32[32,32,128]{2,1,0:T(8,128)S(1)} %get-tuple-element.106.x_ref.a_ref, ...), custom_call_target="tpu_custom_call" | custom-call | tf_op jit(solution)/shard_map/blend/pallas_call | solution.py:436
  91.8 1.7 %blend.2 = (f32[16,64,128]{2,1,0:T(8,128)S(1)}, f32[16,64,128]{2,1,0:T(8,128)S(1)}, f32[64,64]{1,0:T(8,128)S(1)}) custom-call(s32[4]{0:T(128)S(1)} %pad_add_fusion.place_ref, f32[32,64,128]{2,1,0:T(8,128)S(1)} %get-tuple-element.119.refs_3_.x_ref, f32[32,32,128]{2,1,0:T(8,128)S(1)} %get-tuple-element.106.x_ref.a_ref, ...), custom_call_target="tpu_custom_call" | custom-call | tf_op jit(solution)/shard_map/blend/pallas_call | solution.py:436
  94.0 1.5 %collective-permute-done.30.other_ref = f32[16,32,128]{2,1,0:T(8,128)S(1)} collective-permute-done((f32[16,32,128]{2,1,0:T(8,128)S(1)}, f32[16,32,128]{2,1,0:T(8,128)S(1)}, u32[]{:S(2)}, u32[]{:S(2)}) %collective-permute-start.30) | collective-permute-done | bytes 262176 | tf_op jit(solution)/shard_map/ppermute | solution.py:598
  95.5 2.0 %third.1 = (f32[32,64,128]{2,1,0:T(8,128)S(1)}, f32[72,128]{1,0:T(8,128)S(1)}) custom-call(s32[4]{0:T(128)S(1)} %pad_add_fusion.place_ref, f32[16,32,128]{2,1,0:T(8,128)S(1)} %add.57.mine_ref, f32[16,32,128]{2,1,0:T(8,128)S(1)} %collective-permute-done.30.other_ref, f32[64,64]{1,0:T(8,128)S(1)} %get-tuple-element.140.gain_ref, ...), custom_call_target="tpu_custom_call" | custom-call | tf_op jit(solution)/shard_map/third/pallas_call | solution.py:599
  98.8 2.8 %collective-permute-done.31 = f32[72,128]{1,0:T(8,128)S(1)} collective-permute-done((f32[72,128]{1,0:T(8,128)S(1)}, f32[72,128]{1,0:T(8,128)S(1)}, u32[]{:S(2)}, u32[]{:S(2)}) %collective-permute-start.31) | collective-permute-done | bytes 36896 | tf_op jit(solution)/shard_map/ppermute | solution.py:140
  102.7 3.7 %collective-permute-done.32 = f32[72,128]{1,0:T(8,128)S(1)} collective-permute-done((f32[72,128]{1,0:T(8,128)S(1)}, f32[72,128]{1,0:T(8,128)S(1)}, u32[]{:S(2)}, u32[]{:S(2)}) %collective-permute-start.32) | collective-permute-done | bytes 36896 | tf_op jit(solution)/shard_map/ppermute | solution.py:149
  106.4 3.7 %fourth.1 = (f32[64,64]{1,0:T(8,128)S(1)}, f32[64,64]{1,0:T(8,128)S(1)}, f32[64,128]{1,0:T(8,128)S(1)}) custom-call(f32[72,128]{1,0:T(8,128)S(1)} %add.59.gram_ref), custom_call_target="tpu_custom_call" | custom-call | tf_op jit(solution)/shard_map/fourth/pallas_call | solution.py:607
  110.1 1.9 %last.1 = (f32[32,64,128]{2,1,0:T(8,128)}, f32[4,64,64]{2,1,0:T(8,128)}) custom-call(f32[32,64,128]{2,1,0:T(8,128)S(1)} %get-tuple-element.145.w_ref, f32[16,64,128]{2,1,0:T(8,128)S(1)} %get-tuple-element.143.refs_2_.low_ref, f32[16,64,128]{2,1,0:T(8,128)S(1)} %get-tuple-element.144.refs_3_.high_ref, f32[64,128]{1,0:T(8,128)S(1)} %get-tuple-element.147.coef_ref, ...), custom_call_target="tpu_custom_call" | custom-call | tf_op jit(solution)/shard_map/last/pallas_call | solution.py:610
  (86 shorter events, 31.4 us)
Async XLA Ops:
  0.6 8.8 %collective-permute-start.2 = (s32[1,1,44]{2,1,0:T(1,128)}, s32[1,1,44]{2,1,0:T(1,128)S(1)}, u32[]{:S(2)}, u32[]{:S(2)}) collective-permute-start(s32[1,1,44]{2,1,0:T(1,128)} %cols_ref.5), channel_id=1, source_target_pairs={{4,8},{0,12},{8,4},{12,0},{5,9},{1,13},{9,5},{13,1},{6,10},{2,14},... | collective-permute-start | bytes 536 | tf_op jit(solution)/shard_map/ppermute | solution.py:119
  5.8 3.7 %collective-permute-start.1 = (s32[1,1,44]{2,1,0:T(1,128)}, s32[1,1,44]{2,1,0:T(1,128)S(1)}, u32[]{:S(2)}, u32[]{:S(2)}) collective-permute-start(s32[1,1,44]{2,1,0:T(1,128)} %cols_ref.5), channel_id=1, source_target_pairs={{0,4},{8,12},{4,0},{12,8},{1,5},{9,13},{5,1},{13,9},{2,6},{10,14},... | collective-permute-start | bytes 536 | tf_op jit(solution)/shard_map/ppermute | solution.py:119
  5.8 4.6 %collective-permute-start = (s32[1,1,44]{2,1,0:T(1,128)}, s32[1,1,44]{2,1,0:T(1,128)S(1)}, u32[]{:S(2)}, u32[]{:S(2)}) collective-permute-start(s32[1,1,44]{2,1,0:T(1,128)} %cols_ref.5), channel_id=1, source_target_pairs={{0,8},{4,12},{8,0},{12,4},{1,9},{5,13},{9,1},{13,5},{2,10},{6,14},... | collective-permute-start | bytes 536 | tf_op jit(solution)/shard_map/ppermute | solution.py:119
  11.8 6.5 %collective-permute-start.5 = (f32[8,32,128]{2,1,0:T(8,128)S(1)}, f32[8,32,128]{2,1,0:T(8,128)S(1)}, u32[]{:S(2)}, u32[]{:S(2)}) collective-permute-start(f32[8,32,128]{2,1,0:T(8,128)S(1)} %get-tuple-element.82), channel_id=1, source_target_pairs={{0,4},{8,12},{4,0},{12,8},{1,5},{9,13},{5,1},{13,9},{2,6},{10,14},... | collective-permute-start | bytes 393224 | tf_op jit(solution)/shard_map/ppermute | solution.py:119
  13.6 14.3 %collective-permute-start.3 = (f32[8,32,128]{2,1,0:T(8,128)S(1)}, f32[8,32,128]{2,1,0:T(8,128)S(1)}, u32[]{:S(2)}, u32[]{:S(2)}) collective-permute-start(f32[8,32,128]{2,1,0:T(8,128)S(1)} %get-tuple-element.80), channel_id=1, source_target_pairs={{0,8},{4,12},{8,0},{12,4},{1,9},{5,13},{9,1},{13,5},{2,10},{6,14},... | collective-permute-start | bytes 393224 | tf_op jit(solution)/shard_map/ppermute | solution.py:119
  14.6 8.3 %collective-permute-start.4 = (f32[8,32,128]{2,1,0:T(8,128)S(1)}, f32[8,32,128]{2,1,0:T(8,128)S(1)}, u32[]{:S(2)}, u32[]{:S(2)}) collective-permute-start(f32[8,32,128]{2,1,0:T(8,128)S(1)} %get-tuple-element.81), channel_id=1, source_target_pairs={{4,8},{0,12},{8,4},{12,0},{5,9},{1,13},{9,5},{13,1},{6,10},{2,14},... | collective-permute-start | bytes 393224 | tf_op jit(solution)/shard_map/ppermute | solution.py:119
  19.8 8.0 %collective-permute-start.6 = (f32[64,64]{1,0:T(8,128)S(1)}, f32[64,64]{1,0:T(8,128)S(1)}, u32[]{:S(2)}, u32[]{:S(2)}) collective-permute-start(f32[64,64]{1,0:T(8,128)S(1)} %gram.1), channel_id=1, source_target_pairs={{0,4},{4,0},{8,12},{12,8},{1,5},{5,1},{9,13},{13,9},{2,6},{6,2},{1... | collective-permute-start | bytes 49160 | tf_op jit(solution)/shard_map/ppermute | solution.py:140
  23.9 9.5 %collective-permute-start.9 = (f32[8,32,128]{2,1,0:T(8,128)S(1)}, f32[8,32,128]{2,1,0:T(8,128)S(1)}, u32[]{:S(2)}, u32[]{:S(2)}) collective-permute-start(f32[8,32,128]{2,1,0:T(8,128)S(1)} %get-tuple-element.96), channel_id=1, source_target_pairs={{0,4},{8,12},{4,0},{12,8},{1,5},{9,13},{5,1},{13,9},{2,6},{10,14},... | collective-permute-start | bytes 393224 | tf_op jit(solution)/shard_map/ppermute | solution.py:119
  27.8 11.2 %collective-permute-start.10 = (f32[64,64]{1,0:T(8,128)S(1)}, f32[64,64]{1,0:T(8,128)S(1)}, u32[]{:S(2)}, u32[]{:S(2)}) collective-permute-start(f32[64,64]{1,0:T(8,128)S(1)} %add.46), channel_id=1, source_target_pairs={{0,8},{4,12},{8,0},{12,4},{1,9},{5,13},{9,1},{13,5},{2,10},{6,14},... | collective-permute-start | bytes 49160 | tf_op jit(solution)/shard_map/ppermute | solution.py:149
  29.0 14.5 %collective-permute-start.7 = (f32[8,32,128]{2,1,0:T(8,128)S(1)}, f32[8,32,128]{2,1,0:T(8,128)S(1)}, u32[]{:S(2)}, u32[]{:S(2)}) collective-permute-start(f32[8,32,128]{2,1,0:T(8,128)S(1)} %get-tuple-element.93), channel_id=1, source_target_pairs={{0,8},{4,12},{8,0},{12,4},{1,9},{5,13},{9,1},{13,5},{2,10},{6,14},... | collective-permute-start | bytes 393224 | tf_op jit(solution)/shard_map/ppermute | solution.py:119
  31.6 10.5 %collective-permute-start.8 = (f32[8,32,128]{2,1,0:T(8,128)S(1)}, f32[8,32,128]{2,1,0:T(8,128)S(1)}, u32[]{:S(2)}, u32[]{:S(2)}) collective-permute-start(f32[8,32,128]{2,1,0:T(8,128)S(1)} %get-tuple-element.95), channel_id=1, source_target_pairs={{4,8},{0,12},{8,4},{12,0},{5,9},{1,13},{9,5},{13,1},{6,10},{2,14},... | collective-permute-start | bytes 393224 | tf_op jit(solution)/shard_map/ppermute | solution.py:119
  35.0 8.4 %collective-permute-start.13 = (f32[16,32,128]{2,1,0:T(8,128)S(1)}, f32[16,32,128]{2,1,0:T(8,128)S(1)}, u32[]{:S(2)}, u32[]{:S(2)}) collective-permute-start(f32[16,32,128]{2,1,0:T(8,128)S(1)} %add.47), channel_id=1, source_target_pairs={{0,2},{1,3},{2,0},{3,1},{4,6},{5,7},{6,4},{7,5},{8,10},{9,11},{10,... | collective-permute-start | bytes 786440 | tf_op jit(solution)/shard_map/ppermute | solution.py:502
  43.4 1.7 %collective-permute-start.14 = (f32[16,32,128]{2,1,0:T(8,128)S(1)}, f32[16,32,128]{2,1,0:T(8,128)S(1)}, u32[]{:S(2)}, u32[]{:S(2)}) collective-permute-start(f32[16,32,128]{2,1,0:T(8,128)S(1)} %add.49.refs_3_), channel_id=1, source_target_pairs={{0,1},{1,0},{2,3},{3,2},{4,5},{5,4},{6,7},{7,6},{8,9},{9,8},{10,11... | collective-permute-start | bytes 786440 | tf_op jit(solution)/shard_map/ppermute | solution.py:564
  44.6 2.0 %collective-permute-start.12 = (f32[16,32,128]{2,1,0:T(8,128)S(1)}, f32[16,32,128]{2,1,0:T(8,128)S(1)}, u32[]{:S(2)}, u32[]{:S(2)}) collective-permute-start(f32[16,32,128]{2,1,0:T(8,128)S(1)} %get-tuple-element.103), channel_id=1, source_target_pairs={{0,1},{1,0},{2,3},{3,2},{4,5},{5,4},{6,7},{7,6},{8,9},{9,8},{10,11... | collective-permute-start | bytes 786440 | tf_op jit(solution)/shard_map/ppermute | solution.py:568
  46.6 8.3 %collective-permute-start.15 = (f32[16,32,128]{2,1,0:T(8,128)S(1)}, f32[16,32,128]{2,1,0:T(8,128)S(1)}, u32[]{:S(2)}, u32[]{:S(2)}) collective-permute-start(f32[16,32,128]{2,1,0:T(8,128)S(1)} %add.50), channel_id=1, source_target_pairs={{0,2},{1,3},{2,0},{3,1},{4,6},{5,7},{6,4},{7,5},{8,10},{9,11},{10,... | collective-permute-start | bytes 786440 | tf_op jit(solution)/shard_map/ppermute | solution.py:502
  48.2 10.7 %collective-permute-start.17 = (f32[8,32,128]{2,1,0:T(8,128)S(1)}, f32[8,32,128]{2,1,0:T(8,128)S(1)}, u32[]{:S(2)}, u32[]{:S(2)}) collective-permute-start(f32[8,32,128]{2,1,0:T(8,128)S(1)} %get-tuple-element.111), channel_id=1, source_target_pairs={{0,8},{4,12},{8,0},{12,4},{1,9},{5,13},{9,1},{13,5},{2,10},{6,14},... | collective-permute-start | bytes 393224 | tf_op jit(solution)/shard_map/ppermute | solution.py:119
  50.4 12.0 %collective-permute-start.21 = (f32[8,32,128]{2,1,0:T(8,128)S(1)}, f32[8,32,128]{2,1,0:T(8,128)S(1)}, u32[]{:S(2)}, u32[]{:S(2)}) collective-permute-start(f32[8,32,128]{2,1,0:T(8,128)S(1)} %get-tuple-element.120), channel_id=1, source_target_pairs={{0,4},{8,12},{4,0},{12,8},{1,5},{9,13},{5,1},{13,9},{2,6},{10,14},... | collective-permute-start | bytes 393224 | tf_op jit(solution)/shard_map/ppermute | solution.py:119
  51.9 9.5 %collective-permute-start.22 = (f32[8,32,128]{2,1,0:T(8,128)S(1)}, f32[8,32,128]{2,1,0:T(8,128)S(1)}, u32[]{:S(2)}, u32[]{:S(2)}) collective-permute-start(f32[8,32,128]{2,1,0:T(8,128)S(1)} %get-tuple-element.121), channel_id=1, source_target_pairs={{4,8},{0,12},{8,4},{12,0},{5,9},{1,13},{9,5},{13,1},{6,10},{2,14},... | collective-permute-start | bytes 393224 | tf_op jit(solution)/shard_map/ppermute | solution.py:119
  55.0 4.8 %collective-permute-start.16 = (f32[16,32,128]{2,1,0:T(8,128)S(1)}, f32[16,32,128]{2,1,0:T(8,128)S(1)}, u32[]{:S(2)}, u32[]{:S(2)}) collective-permute-start(f32[16,32,128]{2,1,0:T(8,128)S(1)} %add.51.refs_3_), channel_id=1, source_target_pairs={{0,1},{1,0},{2,3},{3,2},{4,5},{5,4},{6,7},{7,6},{8,9},{9,8},{10,11... | collective-permute-start | bytes 786440 | tf_op jit(solution)/shard_map/ppermute | solution.py:572
  61.3 10.4 %collective-permute-start.20 = (f32[8,32,128]{2,1,0:T(8,128)S(1)}, f32[8,32,128]{2,1,0:T(8,128)S(1)}, u32[]{:S(2)}, u32[]{:S(2)}) collective-permute-start(f32[8,32,128]{2,1,0:T(8,128)S(1)} %get-tuple-element.116), channel_id=1, source_target_pairs={{0,4},{8,12},{4,0},{12,8},{1,5},{9,13},{5,1},{13,9},{2,6},{10,14},... | collective-permute-start | bytes 393224 | tf_op jit(solution)/shard_map/ppermute | solution.py:119
  64.6 6.3 %collective-permute-start.24 = (f32[64,128]{1,0:T(8,128)S(1)}, f32[64,128]{1,0:T(8,128)S(1)}, u32[]{:S(2)}, u32[]{:S(2)}) collective-permute-start(f32[64,128]{1,0:T(8,128)S(1)} %cross.1), channel_id=1, source_target_pairs={{0,4},{4,0},{8,12},{12,8},{1,5},{5,1},{9,13},{13,9},{2,6},{6,2},{1... | collective-permute-start | bytes 98312 | tf_op jit(solution)/shard_map/ppermute | solution.py:140
  68.0 14.8 %collective-permute-start.18 = (f32[8,32,128]{2,1,0:T(8,128)S(1)}, f32[8,32,128]{2,1,0:T(8,128)S(1)}, u32[]{:S(2)}, u32[]{:S(2)}) collective-permute-start(f32[8,32,128]{2,1,0:T(8,128)S(1)} %get-tuple-element.114), channel_id=1, source_target_pairs={{0,8},{4,12},{8,0},{12,4},{1,9},{5,13},{9,1},{13,5},{2,10},{6,14},... | collective-permute-start | bytes 393224 | tf_op jit(solution)/shard_map/ppermute | solution.py:119
  68.7 8.3 %collective-permute-start.19 = (f32[8,32,128]{2,1,0:T(8,128)S(1)}, f32[8,32,128]{2,1,0:T(8,128)S(1)}, u32[]{:S(2)}, u32[]{:S(2)}) collective-permute-start(f32[8,32,128]{2,1,0:T(8,128)S(1)} %get-tuple-element.115), channel_id=1, source_target_pairs={{4,8},{0,12},{8,4},{12,0},{5,9},{1,13},{9,5},{13,1},{6,10},{2,14},... | collective-permute-start | bytes 393224 | tf_op jit(solution)/shard_map/ppermute | solution.py:119
  70.8 1.8 %collective-permute-start.23 = (f32[16,32,128]{2,1,0:T(8,128)S(1)}, f32[16,32,128]{2,1,0:T(8,128)S(1)}, u32[]{:S(2)}, u32[]{:S(2)}) collective-permute-start(f32[16,32,128]{2,1,0:T(8,128)S(1)} %get-tuple-element.126), channel_id=1, source_target_pairs={{0,1},{1,0},{2,3},{3,2},{4,5},{5,4},{6,7},{7,6},{8,9},{9,8},{10,11... | collective-permute-start | bytes 786440 | tf_op jit(solution)/shard_map/ppermute | solution.py:578
  70.8 12.0 %collective-permute-start.25 = (f32[64,128]{1,0:T(8,128)S(1)}, f32[64,128]{1,0:T(8,128)S(1)}, u32[]{:S(2)}, u32[]{:S(2)}) collective-permute-start(f32[64,128]{1,0:T(8,128)S(1)} %add.53), channel_id=1, source_target_pairs={{0,8},{4,12},{8,0},{12,4},{1,9},{5,13},{9,1},{13,5},{2,10},{6,14},... | collective-permute-start | bytes 98312 | tf_op jit(solution)/shard_map/ppermute | solution.py:149
  72.7 11.2 %collective-permute-start.27 = (f32[16,32,128]{2,1,0:T(8,128)S(1)}, f32[16,32,128]{2,1,0:T(8,128)S(1)}, u32[]{:S(2)}, u32[]{:S(2)}) collective-permute-start(f32[16,32,128]{2,1,0:T(8,128)S(1)} %add.52), channel_id=1, source_target_pairs={{0,2},{1,3},{2,0},{3,1},{4,6},{5,7},{6,4},{7,5},{8,10},{9,11},{10,... | collective-permute-start | bytes 786440 | tf_op jit(solution)/shard_map/ppermute | solution.py:502
  83.8 1.6 %collective-permute-start.26 = (f32[16,32,128]{2,1,0:T(8,128)S(1)}, f32[16,32,128]{2,1,0:T(8,128)S(1)}, u32[]{:S(2)}, u32[]{:S(2)}) collective-permute-start(f32[16,32,128]{2,1,0:T(8,128)S(1)} %get-tuple-element.132), channel_id=1, source_target_pairs={{0,1},{1,0},{2,3},{3,2},{4,5},{5,4},{6,7},{7,6},{8,9},{9,8},{10,11... | collective-permute-start | bytes 786440 | tf_op jit(solution)/shard_map/ppermute | solution.py:590
  84.0 6.1 %collective-permute-start.29 = (f32[16,32,128]{2,1,0:T(8,128)S(1)}, f32[16,32,128]{2,1,0:T(8,128)S(1)}, u32[]{:S(2)}, u32[]{:S(2)}) collective-permute-start(f32[16,32,128]{2,1,0:T(8,128)S(1)} %add.55.mine_ref), channel_id=1, source_target_pairs={{0,1},{1,0},{2,3},{3,2},{4,5},{5,4},{6,7},{7,6},{8,9},{9,8},{10,11... | collective-permute-start | bytes 786440 | tf_op jit(solution)/shard_map/ppermute | solution.py:589
  85.5 8.4 %collective-permute-start.28 = (f32[16,32,128]{2,1,0:T(8,128)S(1)}, f32[16,32,128]{2,1,0:T(8,128)S(1)}, u32[]{:S(2)}, u32[]{:S(2)}) collective-permute-start(f32[16,32,128]{2,1,0:T(8,128)S(1)} %add.56), channel_id=1, source_target_pairs={{0,2},{1,3},{2,0},{3,1},{4,6},{5,7},{6,4},{7,5},{8,10},{9,11},{10,... | collective-permute-start | bytes 786440 | tf_op jit(solution)/shard_map/ppermute | solution.py:502
  93.9 1.6 %collective-permute-start.30 = (f32[16,32,128]{2,1,0:T(8,128)S(1)}, f32[16,32,128]{2,1,0:T(8,128)S(1)}, u32[]{:S(2)}, u32[]{:S(2)}) collective-permute-start(f32[16,32,128]{2,1,0:T(8,128)S(1)} %add.57.mine_ref), channel_id=1, source_target_pairs={{0,1},{1,0},{2,3},{3,2},{4,5},{5,4},{6,7},{7,6},{8,9},{9,8},{10,11... | collective-permute-start | bytes 786440 | tf_op jit(solution)/shard_map/ppermute | solution.py:598
  97.6 4.0 %collective-permute-start.31 = (f32[72,128]{1,0:T(8,128)S(1)}, f32[72,128]{1,0:T(8,128)S(1)}, u32[]{:S(2)}, u32[]{:S(2)}) collective-permute-start(f32[72,128]{1,0:T(8,128)S(1)} %get-tuple-element.146), channel_id=1, source_target_pairs={{0,4},{4,0},{8,12},{12,8},{1,5},{5,1},{9,13},{13,9},{2,6},{6,2},{1... | collective-permute-start | bytes 110600 | tf_op jit(solution)/shard_map/ppermute | solution.py:140
  101.6 4.9 %collective-permute-start.32 = (f32[72,128]{1,0:T(8,128)S(1)}, f32[72,128]{1,0:T(8,128)S(1)}, u32[]{:S(2)}, u32[]{:S(2)}) collective-permute-start(f32[72,128]{1,0:T(8,128)S(1)} %add.58), channel_id=1, source_target_pairs={{0,8},{4,12},{8,0},{12,4},{1,9},{5,13},{9,1},{13,5},{2,10},{6,14},... | collective-permute-start | bytes 110600 | tf_op jit(solution)/shard_map/ppermute | solution.py:149
  (5 other events, 29.4 us)

commit v13 on v11

--- a/solution.py
+++ b/solution.py
@@ -151,8 +151,21 @@
     return block
 
 
-def all_sum(block, axis, *tokens):
-    return end_sum(start_sum(block, axis), axis, *tokens)
+def all_sum(block, axis):
+    size = lax.axis_size(axis)
+    if size & (size - 1):
+        return lax.psum(block, axis)
+    step = 1
+    while step < size:
+        masks = [step] if 2 * step >= size else [step, 2 * step, 3 * step]
+        got = [lax.ppermute(block, axis, [(i, i ^ m) for i in range(size)]) for m in masks]
+        if len(got) == 1:
+            block = block + got[0]
+            step *= 2
+        else:
+            block = (block + got[0]) + (got[1] + got[2])
+            step *= 4
+    return block
 
 
 def factor(gram):
@@ -576,19 +589,19 @@
     keep_a, give_a = join(acc_a, got_a, groups[0], last=True)
 
     core = lax.ppermute(give_a, "vec", swap)
+    (acc_b,) = own(after(y_b, keep_a), acc_b)
     acc_b = join(acc_b, got_b, groups[0])
     mine_a = keep_a + after(core, acc_b)
     (gram,) = call(cross_body, [(width, 2 * width)], [VMEM] * 3, name="cross")(x, y_a, after(y_b, mine_a))
-    (acc_b,) = own(y_b, after(acc_b, gram))
-    acc_b = join(acc_b, got_b, groups[1])
+    acc_b = join(after(acc_b, gram), got_b, groups[1])
     cross_gram = start_sum(gram, "res")
     keep_b, give_b = join(after(acc_b, cross_gram), got_b, groups[2], last=True)
 
     core = lax.ppermute(give_b, "vec", swap)
     mine_a = across(mine_a, cross_gram)
     other_a = lax.ppermute(mine_a, "vec", swap)
-    cross_gram = end_sum(cross_gram, "res")
-    mine_b = keep_b + after(core, mine_a, cross_gram)
+    mine_b = keep_b + after(core, mine_a)
+    cross_gram = end_sum(cross_gram, "res", mine_b)
     cross1, lower1, coef, gain = call(
         second_body, [square, square, (2 * width, 3 * width), square], [VMEM] * 2, name="second"
     )(after(cross_gram, mine_b), start_inv)

time: 112 us -> 110 us (0.982)
  waiting for transfers between devices: 28.6 us -> 24.6 us
  starting transfers between devices: 37.2 us -> 39.8 us
    ppermute x3 -> x2, waiting for transfers between devices: 10.9 us -> 5.97 us  [end_sum(): got = lax.ppermute(block, axis, [(i, i ^ step) for i in range(size)])]
    ppermute x0 -> x3, starting transfers between devices: none -> 4.42 us  [all_sum(): lax.ppermute(block, axis, [(i, i ^ m) for i in range(size)])]
    ppermute x15, waiting for transfers between devices: 11.6 us -> 7.57 us  [exchange(): lax.ppermute(block, axis, [(a, b) for a, b in pairs] + [(b, a) for a, b i...]
    ppermute x0 -> x3, waiting for transfers between devices: none -> 3.09 us  [all_sum(): lax.ppermute(block, axis, [(i, i ^ m) for i in range(size)])]
    ppermute x4, waiting for transfers between devices: 1.41 us -> 4.25 us  [across(): got = lax.ppermute(mine, 'vec', [(i, i ^ step) for i in range(lanes)])]
    ppermute x3 -> x2, starting transfers between devices: 3.26 us -> 1.54 us  [start_sum(): lax.ppermute(block, axis, [(i, i ^ step) for i in range(size)])]
    ppermute x3 -> x2, waiting for transfers between devices: 2.56 us -> 1.59 us  [start_sum(): lax.ppermute(block, axis, [(i, i ^ step) for i in range(size)])]
  transfers between devices with their start and end apart: 33 -> 34, of which waited for: 14 -> 15; matrix products, arithmetic and copies ran while one was open for 1% -> 1% of each run, Pallas kernels for 31% -> 31%
where the time goes in v13:
time: 110 us
  Pallas kernels  43.5 us (40%)
  starting transfers between devices  39.8 us (36%)
  waiting for transfers between devices  24.6 us (22%)
    ppermute x15, starting transfers between devices, exchange(): lax.ppermute(block, axis, [(a, b) for a, b in pairs] + [(b, a) for a, b i...  27.2 us
    pallas_call x12, Pallas kernels, join(): call(body, [halfchunk] * 2 if last else [chunk], [SMEM] * (3 + size) + [V...  11.9 us
    ppermute x15, waiting for transfers between devices, exchange(): lax.ppermute(block, axis, [(a, b) for a, b in pairs] + [(b, a) for a, b i...  7.57 us
    ppermute x2, waiting for transfers between devices, end_sum(): got = lax.ppermute(block, axis, [(i, i ^ step) for i in range(size)])  5.97 us
    pallas_call x3, Pallas kernels, own(): call(own_body, [chunk] * len(accs), [SMEM] * 2 + [VMEM] * (2 + len(accs))...  5.46 us
    ppermute x3, starting transfers between devices, all_sum(): lax.ppermute(block, axis, [(i, i ^ m) for i in range(size)])  4.42 us
    ppermute x4, starting transfers between devices, across(): got = lax.ppermute(mine, 'vec', [(i, i ^ step) for i in range(lanes)])  4.32 us
    ppermute x4, waiting for transfers between devices, across(): got = lax.ppermute(mine, 'vec', [(i, i ^ step) for i in range(lanes)])  4.25 us
  transfers between devices with their start and end apart: 34, of which 15 were waited for; matrix products, arithmetic and copies ran while one was open for 1% of the time, Pallas kernels for 31%

profile of v13, /device:TPU:0, one launch (start us, length us, event | category | flops | bytes accessed | tf_op | source)
XLA Modules:
  0.0 110.0 jit_solution(7719179386286941697)
XLA Ops:
  0.6 5.1 %collective-permute-start.2 = (s32[1,1,44]{2,1,0:T(1,128)}, s32[1,1,44]{2,1,0:T(1,128)S(1)}, u32[]{:S(2)}, u32[]{:S(2)}) collective-permute-start(s32[1,1,44]{2,1,0:T(1,128)} %cols_ref.5), channel_id=1, source_target_pairs={{4,8},{0,12},{8,4},{12,0},{5,9},{1,13},{9,5},{13,1},{6,10},{2,14},... | collective-permute-start | bytes 536 | tf_op jit(solution)/shard_map/ppermute | solution.py:119
  7.2 2.3 %prepare.1 = (f32[32,64,128]{2,1,0:T(8,128)S(1)}, bf16[44,2,128,128]{3,2,1,0:T(8,128)(2,1)S(1)}, f32[32,32,128]{2,1,0:T(8,128)S(1)}, f32[32,32,128]{2,1,0:T(8,128)S(1)}) custom-call(f32[32,64,128]{2,1,0:T(8,128)} %x_hbm.1, f32[32,128]{1,0:T(8,128)} %refs_5_.3, f32[1,1,44,128,128]{4,3,2,1,0:T(8,128)} %tiles_hbm.1), custom_call_target="tpu_custom_call" | custom-call | tf_op jit(solution)/shard_map/prepare/pallas_call | solution.py:539
  11.8 1.8 %collective-permute-start.5 = (f32[8,32,128]{2,1,0:T(8,128)S(1)}, f32[8,32,128]{2,1,0:T(8,128)S(1)}, u32[]{:S(2)}, u32[]{:S(2)}) collective-permute-start(f32[8,32,128]{2,1,0:T(8,128)S(1)} %get-tuple-element.82), channel_id=1, source_target_pairs={{0,4},{8,12},{4,0},{12,8},{1,5},{9,13},{5,1},{13,9},{2,6},{10,14},... | collective-permute-start | bytes 393224 | tf_op jit(solution)/shard_map/ppermute | solution.py:119
  14.6 1.6 %collective-permute-start.4 = (f32[8,32,128]{2,1,0:T(8,128)S(1)}, f32[8,32,128]{2,1,0:T(8,128)S(1)}, u32[]{:S(2)}, u32[]{:S(2)}) collective-permute-start(f32[8,32,128]{2,1,0:T(8,128)S(1)} %get-tuple-element.81), channel_id=1, source_target_pairs={{4,8},{0,12},{8,4},{12,0},{5,9},{1,13},{9,5},{13,1},{6,10},{2,14},... | collective-permute-start | bytes 393224 | tf_op jit(solution)/shard_map/ppermute | solution.py:119
  16.2 2.0 %own.3 = (f32[32,32,128]{2,1,0:T(8,128)S(1)}, f32[32,32,128]{2,1,0:T(8,128)S(1)}) custom-call(s32[1,1,44]{2,1,0:T(1,128)S(1)} %copy-done.1, s32[1,1,44]{2,1,0:T(1,128)S(1)} %copy-done.2, f32[32,64,128]{2,1,0:T(8,128)S(1)} %get-tuple-element.124.refs_3_.x_ref, ...), custom_call_target="tpu_custom_call", output_to_operand_aliasing={{0}: (4, {}), {1}: (5, {})} | custom-call | tf_op jit(solution)/shard_map/own/pallas_call | solution.py:530
  21.2 1.7 %collective-permute-done.4.refs_1_ = f32[8,32,128]{2,1,0:T(8,128)S(1)} collective-permute-done((f32[8,32,128]{2,1,0:T(8,128)S(1)}, f32[8,32,128]{2,1,0:T(8,128)S(1)}, u32[]{:S(2)}, u32[]{:S(2)}) %collective-permute-start.4) | collective-permute-done | bytes 131104 | tf_op jit(solution)/shard_map/ppermute | solution.py:119
  23.9 3.9 %collective-permute-start.9 = (f32[8,32,128]{2,1,0:T(8,128)S(1)}, f32[8,32,128]{2,1,0:T(8,128)S(1)}, u32[]{:S(2)}, u32[]{:S(2)}) collective-permute-start(f32[8,32,128]{2,1,0:T(8,128)S(1)} %get-tuple-element.96), channel_id=1, source_target_pairs={{0,4},{8,12},{4,0},{12,8},{1,5},{9,13},{5,1},{13,9},{2,6},{10,14},... | collective-permute-start | bytes 393224 | tf_op jit(solution)/shard_map/ppermute | solution.py:119
  29.0 2.6 %collective-permute-start.7 = (f32[8,32,128]{2,1,0:T(8,128)S(1)}, f32[8,32,128]{2,1,0:T(8,128)S(1)}, u32[]{:S(2)}, u32[]{:S(2)}) collective-permute-start(f32[8,32,128]{2,1,0:T(8,128)S(1)} %get-tuple-element.93), channel_id=1, source_target_pairs={{0,8},{4,12},{8,0},{12,4},{1,9},{5,13},{9,1},{13,5},{2,10},{6,14},... | collective-permute-start | bytes 393224 | tf_op jit(solution)/shard_map/ppermute | solution.py:119
  31.6 1.9 %collective-permute-start.8 = (f32[8,32,128]{2,1,0:T(8,128)S(1)}, f32[8,32,128]{2,1,0:T(8,128)S(1)}, u32[]{:S(2)}, u32[]{:S(2)}) collective-permute-start(f32[8,32,128]{2,1,0:T(8,128)S(1)} %get-tuple-element.95), channel_id=1, source_target_pairs={{4,8},{0,12},{8,4},{12,0},{5,9},{1,13},{9,5},{13,1},{6,10},{2,14},... | collective-permute-start | bytes 393224 | tf_op jit(solution)/shard_map/ppermute | solution.py:119
  35.0 1.6 %collective-permute-start.13 = (f32[16,32,128]{2,1,0:T(8,128)S(1)}, f32[16,32,128]{2,1,0:T(8,128)S(1)}, u32[]{:S(2)}, u32[]{:S(2)}) collective-permute-start(f32[16,32,128]{2,1,0:T(8,128)S(1)} %add.50), channel_id=1, source_target_pairs={{0,2},{1,3},{2,0},{3,1},{4,6},{5,7},{6,4},{7,5},{8,10},{9,11},{10,... | collective-permute-start | bytes 786440 | tf_op jit(solution)/shard_map/ppermute | solution.py:515
  36.5 2.5 %collective-permute-done.10 = f32[64,64]{1,0:T(8,128)S(1)} collective-permute-done((f32[64,64]{1,0:T(8,128)S(1)}, f32[64,64]{1,0:T(8,128)S(1)}, u32[]{:S(2)}, u32[]{:S(2)}) %collective-permute-start.10) | collective-permute-done | bytes 16416 | tf_op jit(solution)/shard_map/ppermute | solution.py:149
  39.0 3.0 %first.1.inverse_ref = f32[64,64]{1,0:T(8,128)S(1)} custom-call(f32[64,64]{1,0:T(8,128)S(1)} %add.51.gram_ref), custom_call_target="tpu_custom_call" | custom-call | tf_op jit(solution)/shard_map/first/pallas_call | solution.py:574
  46.6 1.6 %collective-permute-start.15 = (f32[16,32,128]{2,1,0:T(8,128)S(1)}, f32[16,32,128]{2,1,0:T(8,128)S(1)}, u32[]{:S(2)}, u32[]{:S(2)}) collective-permute-start(f32[16,32,128]{2,1,0:T(8,128)S(1)} %add.53), channel_id=1, source_target_pairs={{0,2},{1,3},{2,0},{3,1},{4,6},{5,7},{6,4},{7,5},{8,10},{9,11},{10,... | collective-permute-start | bytes 786440 | tf_op jit(solution)/shard_map/ppermute | solution.py:515
  48.6 1.7 %own.4.refs_3_ = f32[32,32,128]{2,1,0:T(8,128)S(1)} custom-call(s32[1,1,44]{2,1,0:T(1,128)S(1)} %copy-done.1, s32[1,1,44]{2,1,0:T(1,128)S(1)} %copy-done.2, f32[32,32,128]{2,1,0:T(8,128)S(1)} %get-tuple-element.106.x_ref.a_ref, bf16[44,2,128,128]{3,2,1,0:T(8,128)(2,1)S(1)} %get-tuple-element.78.refs_4_.split_ref.refs_2_.refs_6_, ...), custom_call_target="tpu_custom_call", output_to_operand_aliasing={{}: (4, {})} | custom-call | tf_op jit(solution)/shard_map/own/pallas_call | solution.py:530
  50.4 1.5 %collective-permute-start.21 = (f32[8,32,128]{2,1,0:T(8,128)S(1)}, f32[8,32,128]{2,1,0:T(8,128)S(1)}, u32[]{:S(2)}, u32[]{:S(2)}) collective-permute-start(f32[8,32,128]{2,1,0:T(8,128)S(1)} %get-tuple-element.118), channel_id=1, source_target_pairs={{0,4},{8,12},{4,0},{12,8},{1,5},{9,13},{5,1},{13,9},{2,6},{10,14},... | collective-permute-start | bytes 393224 | tf_op jit(solution)/shard_map/ppermute | solution.py:119
  51.9 2.5 %collective-permute-start.22 = (f32[8,32,128]{2,1,0:T(8,128)S(1)}, f32[8,32,128]{2,1,0:T(8,128)S(1)}, u32[]{:S(2)}, u32[]{:S(2)}) collective-permute-start(f32[8,32,128]{2,1,0:T(8,128)S(1)} %get-tuple-element.119), channel_id=1, source_target_pairs={{4,8},{0,12},{8,4},{12,0},{5,9},{1,13},{9,5},{13,1},{6,10},{2,14},... | collective-permute-start | bytes 393224 | tf_op jit(solution)/shard_map/ppermute | solution.py:119
  55.1 3.8 %collective-permute-done.17.refs_1_ = f32[8,32,128]{2,1,0:T(8,128)S(1)} collective-permute-done((f32[8,32,128]{2,1,0:T(8,128)S(1)}, f32[8,32,128]{2,1,0:T(8,128)S(1)}, u32[]{:S(2)}, u32[]{:S(2)}) %collective-permute-start.17) | collective-permute-done | bytes 131104 | tf_op jit(solution)/shard_map/ppermute | solution.py:119
  63.5 1.7 %collective-permute-start.18 = (f32[8,32,128]{2,1,0:T(8,128)S(1)}, f32[8,32,128]{2,1,0:T(8,128)S(1)}, u32[]{:S(2)}, u32[]{:S(2)}) collective-permute-start(f32[8,32,128]{2,1,0:T(8,128)S(1)} %get-tuple-element.114), channel_id=1, source_target_pairs={{0,8},{4,12},{8,0},{12,4},{1,9},{5,13},{9,1},{13,5},{2,10},{6,14},... | collective-permute-start | bytes 393224 | tf_op jit(solution)/shard_map/ppermute | solution.py:119
  65.3 2.4 %collective-permute-start.19 = (f32[8,32,128]{2,1,0:T(8,128)S(1)}, f32[8,32,128]{2,1,0:T(8,128)S(1)}, u32[]{:S(2)}, u32[]{:S(2)}) collective-permute-start(f32[8,32,128]{2,1,0:T(8,128)S(1)} %get-tuple-element.115), channel_id=1, source_target_pairs={{4,8},{0,12},{8,4},{12,0},{5,9},{1,13},{9,5},{13,1},{6,10},{2,14},... | collective-permute-start | bytes 393224 | tf_op jit(solution)/shard_map/ppermute | solution.py:119
  67.6 1.7 %own.5.refs_3_ = f32[32,32,128]{2,1,0:T(8,128)S(1)} custom-call(s32[1,1,44]{2,1,0:T(1,128)S(1)} %copy-done.1, s32[1,1,44]{2,1,0:T(1,128)S(1)} %copy-done.2, f32[32,32,128]{2,1,0:T(8,128)S(1)} %get-tuple-element.127.x_ref.b_ref, bf16[44,2,128,128]{3,2,1,0:T(8,128)(2,1)S(1)} %get-tuple-element.78.refs_4_.split_ref.refs_2_.refs_6_, ...), custom_call_target="tpu_custom_call", output_to_operand_aliasing={{}: (4, {})} | custom-call | tf_op jit(solution)/shard_map/own/pallas_call | solution.py:530
  74.3 1.6 %collective-permute-done.24 = f32[64,128]{1,0:T(8,128)S(1)} collective-permute-done((f32[64,128]{1,0:T(8,128)S(1)}, f32[64,128]{1,0:T(8,128)S(1)}, u32[]{:S(2)}, u32[]{:S(2)}) %collective-permute-start.24) | collective-permute-done | bytes 32800 | tf_op jit(solution)/shard_map/ppermute | solution.py:140
  77.1 3.2 %collective-permute-done.26 = f32[16,32,128]{2,1,0:T(8,128)S(1)} collective-permute-done((f32[16,32,128]{2,1,0:T(8,128)S(1)}, f32[16,32,128]{2,1,0:T(8,128)S(1)}, u32[]{:S(2)}, u32[]{:S(2)}) %collective-permute-start.26) | collective-permute-done | bytes 262176 | tf_op jit(solution)/shard_map/ppermute | solution.py:515
  82.4 3.5 %collective-permute-done.29 = f32[64,128]{1,0:T(8,128)S(1)} collective-permute-done((f32[64,128]{1,0:T(8,128)S(1)}, f32[64,128]{1,0:T(8,128)S(1)}, u32[]{:S(2)}, u32[]{:S(2)}) %collective-permute-start.29) | collective-permute-done | bytes 32800 | tf_op jit(solution)/shard_map/ppermute | solution.py:149
  85.9 3.9 %second.1 = (f32[64,64]{1,0:T(8,128)S(1)}, f32[64,64]{1,0:T(8,128)S(1)}, f32[128,192]{1,0:T(8,128)S(1)}, f32[64,64]{1,0:T(8,128)S(1)}) custom-call(f32[64,128]{1,0:T(8,128)S(1)} %add.59.gram_ref, f32[64,64]{1,0:T(8,128)S(1)} %first.1.inverse_ref), custom_call_target="tpu_custom_call" | custom-call | tf_op jit(solution)/shard_map/second/pallas_call | solution.py:605
  89.8 1.7 %blend.3 = (f32[16,64,128]{2,1,0:T(8,128)S(1)}, f32[16,64,128]{2,1,0:T(8,128)S(1)}, f32[64,64]{1,0:T(8,128)S(1)}) custom-call(s32[4]{0:T(128)S(1)} %pad_add_fusion.place_ref, f32[32,64,128]{2,1,0:T(8,128)S(1)} %get-tuple-element.124.refs_3_.x_ref, f32[32,32,128]{2,1,0:T(8,128)S(1)} %get-tuple-element.106.x_ref.a_ref, ...), custom_call_target="tpu_custom_call" | custom-call | tf_op jit(solution)/shard_map/blend/pallas_call | solution.py:449
  91.6 1.7 %blend.2 = (f32[16,64,128]{2,1,0:T(8,128)S(1)}, f32[16,64,128]{2,1,0:T(8,128)S(1)}, f32[64,64]{1,0:T(8,128)S(1)}) custom-call(s32[4]{0:T(128)S(1)} %pad_add_fusion.place_ref, f32[32,64,128]{2,1,0:T(8,128)S(1)} %get-tuple-element.124.refs_3_.x_ref, f32[32,32,128]{2,1,0:T(8,128)S(1)} %get-tuple-element.106.x_ref.a_ref, ...), custom_call_target="tpu_custom_call" | custom-call | tf_op jit(solution)/shard_map/blend/pallas_call | solution.py:449
  93.4 1.5 %collective-permute-done.30.other_ref = f32[16,32,128]{2,1,0:T(8,128)S(1)} collective-permute-done((f32[16,32,128]{2,1,0:T(8,128)S(1)}, f32[16,32,128]{2,1,0:T(8,128)S(1)}, u32[]{:S(2)}, u32[]{:S(2)}) %collective-permute-start.30) | collective-permute-done | bytes 262176 | tf_op jit(solution)/shard_map/ppermute | solution.py:611
  94.9 2.0 %third.1 = (f32[32,64,128]{2,1,0:T(8,128)S(1)}, f32[72,128]{1,0:T(8,128)S(1)}) custom-call(s32[4]{0:T(128)S(1)} %pad_add_fusion.place_ref, f32[16,32,128]{2,1,0:T(8,128)S(1)} %add.60.mine_ref, f32[16,32,128]{2,1,0:T(8,128)S(1)} %collective-permute-done.30.other_ref, f32[64,64]{1,0:T(8,128)S(1)} %get-tuple-element.140.gain_ref, ...), custom_call_target="tpu_custom_call" | custom-call | tf_op jit(solution)/shard_map/third/pallas_call | solution.py:612
  98.1 2.0 %collective-permute-start.32 = (f32[72,128]{1,0:T(8,128)S(1)}, f32[72,128]{1,0:T(8,128)S(1)}, u32[]{:S(2)}, u32[]{:S(2)}) collective-permute-start(f32[72,128]{1,0:T(8,128)S(1)} %get-tuple-element.146), channel_id=1, source_target_pairs={{0,8},{4,12},{8,0},{12,4},{1,9},{5,13},{9,1},{13,5},{2,10},{6,14},... | collective-permute-start | bytes 110600 | tf_op jit(solution)/shard_map/ppermute | solution.py:161
  101.4 1.6 %collective-permute-done.33 = f32[72,128]{1,0:T(8,128)S(1)} collective-permute-done((f32[72,128]{1,0:T(8,128)S(1)}, f32[72,128]{1,0:T(8,128)S(1)}, u32[]{:S(2)}, u32[]{:S(2)}) %collective-permute-start.33) | collective-permute-done | bytes 36896 | tf_op jit(solution)/shard_map/ppermute | solution.py:161
  104.5 3.7 %fourth.1 = (f32[64,64]{1,0:T(8,128)S(1)}, f32[64,64]{1,0:T(8,128)S(1)}, f32[64,128]{1,0:T(8,128)S(1)}) custom-call(f32[72,128]{1,0:T(8,128)S(1)} %add_add_fusion.gram_ref), custom_call_target="tpu_custom_call" | custom-call | tf_op jit(solution)/shard_map/fourth/pallas_call | solution.py:620
  108.2 1.9 %last.1 = (f32[32,64,128]{2,1,0:T(8,128)}, f32[4,64,64]{2,1,0:T(8,128)}) custom-call(f32[32,64,128]{2,1,0:T(8,128)S(1)} %get-tuple-element.145.w_ref, f32[16,64,128]{2,1,0:T(8,128)S(1)} %get-tuple-element.143.refs_2_.low_ref, f32[16,64,128]{2,1,0:T(8,128)S(1)} %get-tuple-element.144.refs_3_.high_ref, f32[64,128]{1,0:T(8,128)S(1)} %get-tuple-element.147.coef_ref, ...), custom_call_target="tpu_custom_call" | custom-call | tf_op jit(solution)/shard_map/last/pallas_call | solution.py:623
  (87 shorter events, 33.8 us)
Async XLA Ops:
  0.6 8.8 %collective-permute-start.2 = (s32[1,1,44]{2,1,0:T(1,128)}, s32[1,1,44]{2,1,0:T(1,128)S(1)}, u32[]{:S(2)}, u32[]{:S(2)}) collective-permute-start(s32[1,1,44]{2,1,0:T(1,128)} %cols_ref.5), channel_id=1, source_target_pairs={{4,8},{0,12},{8,4},{12,0},{5,9},{1,13},{9,5},{13,1},{6,10},{2,14},... | collective-permute-start | bytes 536 | tf_op jit(solution)/shard_map/ppermute | solution.py:119
  5.8 3.7 %collective-permute-start.1 = (s32[1,1,44]{2,1,0:T(1,128)}, s32[1,1,44]{2,1,0:T(1,128)S(1)}, u32[]{:S(2)}, u32[]{:S(2)}) collective-permute-start(s32[1,1,44]{2,1,0:T(1,128)} %cols_ref.5), channel_id=1, source_target_pairs={{0,4},{8,12},{4,0},{12,8},{1,5},{9,13},{5,1},{13,9},{2,6},{10,14},... | collective-permute-start | bytes 536 | tf_op jit(solution)/shard_map/ppermute | solution.py:119
  5.8 4.6 %collective-permute-start = (s32[1,1,44]{2,1,0:T(1,128)}, s32[1,1,44]{2,1,0:T(1,128)S(1)}, u32[]{:S(2)}, u32[]{:S(2)}) collective-permute-start(s32[1,1,44]{2,1,0:T(1,128)} %cols_ref.5), channel_id=1, source_target_pairs={{0,8},{4,12},{8,0},{12,4},{1,9},{5,13},{9,1},{13,5},{2,10},{6,14},... | collective-permute-start | bytes 536 | tf_op jit(solution)/shard_map/ppermute | solution.py:119
  11.8 6.5 %collective-permute-start.5 = (f32[8,32,128]{2,1,0:T(8,128)S(1)}, f32[8,32,128]{2,1,0:T(8,128)S(1)}, u32[]{:S(2)}, u32[]{:S(2)}) collective-permute-start(f32[8,32,128]{2,1,0:T(8,128)S(1)} %get-tuple-element.82), channel_id=1, source_target_pairs={{0,4},{8,12},{4,0},{12,8},{1,5},{9,13},{5,1},{13,9},{2,6},{10,14},... | collective-permute-start | bytes 393224 | tf_op jit(solution)/shard_map/ppermute | solution.py:119
  13.6 14.3 %collective-permute-start.3 = (f32[8,32,128]{2,1,0:T(8,128)S(1)}, f32[8,32,128]{2,1,0:T(8,128)S(1)}, u32[]{:S(2)}, u32[]{:S(2)}) collective-permute-start(f32[8,32,128]{2,1,0:T(8,128)S(1)} %get-tuple-element.80), channel_id=1, source_target_pairs={{0,8},{4,12},{8,0},{12,4},{1,9},{5,13},{9,1},{13,5},{2,10},{6,14},... | collective-permute-start | bytes 393224 | tf_op jit(solution)/shard_map/ppermute | solution.py:119
  14.6 8.3 %collective-permute-start.4 = (f32[8,32,128]{2,1,0:T(8,128)S(1)}, f32[8,32,128]{2,1,0:T(8,128)S(1)}, u32[]{:S(2)}, u32[]{:S(2)}) collective-permute-start(f32[8,32,128]{2,1,0:T(8,128)S(1)} %get-tuple-element.81), channel_id=1, source_target_pairs={{4,8},{0,12},{8,4},{12,0},{5,9},{1,13},{9,5},{13,1},{6,10},{2,14},... | collective-permute-start | bytes 393224 | tf_op jit(solution)/shard_map/ppermute | solution.py:119
  19.8 8.0 %collective-permute-start.6 = (f32[64,64]{1,0:T(8,128)S(1)}, f32[64,64]{1,0:T(8,128)S(1)}, u32[]{:S(2)}, u32[]{:S(2)}) collective-permute-start(f32[64,64]{1,0:T(8,128)S(1)} %gram.1), channel_id=1, source_target_pairs={{0,4},{4,0},{8,12},{12,8},{1,5},{5,1},{9,13},{13,9},{2,6},{6,2},{1... | collective-permute-start | bytes 49160 | tf_op jit(solution)/shard_map/ppermute | solution.py:140
  23.9 9.5 %collective-permute-start.9 = (f32[8,32,128]{2,1,0:T(8,128)S(1)}, f32[8,32,128]{2,1,0:T(8,128)S(1)}, u32[]{:S(2)}, u32[]{:S(2)}) collective-permute-start(f32[8,32,128]{2,1,0:T(8,128)S(1)} %get-tuple-element.96), channel_id=1, source_target_pairs={{0,4},{8,12},{4,0},{12,8},{1,5},{9,13},{5,1},{13,9},{2,6},{10,14},... | collective-permute-start | bytes 393224 | tf_op jit(solution)/shard_map/ppermute | solution.py:119
  27.8 11.2 %collective-permute-start.10 = (f32[64,64]{1,0:T(8,128)S(1)}, f32[64,64]{1,0:T(8,128)S(1)}, u32[]{:S(2)}, u32[]{:S(2)}) collective-permute-start(f32[64,64]{1,0:T(8,128)S(1)} %add.49), channel_id=1, source_target_pairs={{0,8},{4,12},{8,0},{12,4},{1,9},{5,13},{9,1},{13,5},{2,10},{6,14},... | collective-permute-start | bytes 49160 | tf_op jit(solution)/shard_map/ppermute | solution.py:149
  29.0 14.6 %collective-permute-start.7 = (f32[8,32,128]{2,1,0:T(8,128)S(1)}, f32[8,32,128]{2,1,0:T(8,128)S(1)}, u32[]{:S(2)}, u32[]{:S(2)}) collective-permute-start(f32[8,32,128]{2,1,0:T(8,128)S(1)} %get-tuple-element.93), channel_id=1, source_target_pairs={{0,8},{4,12},{8,0},{12,4},{1,9},{5,13},{9,1},{13,5},{2,10},{6,14},... | collective-permute-start | bytes 393224 | tf_op jit(solution)/shard_map/ppermute | solution.py:119
  31.6 10.5 %collective-permute-start.8 = (f32[8,32,128]{2,1,0:T(8,128)S(1)}, f32[8,32,128]{2,1,0:T(8,128)S(1)}, u32[]{:S(2)}, u32[]{:S(2)}) collective-permute-start(f32[8,32,128]{2,1,0:T(8,128)S(1)} %get-tuple-element.95), channel_id=1, source_target_pairs={{4,8},{0,12},{8,4},{12,0},{5,9},{1,13},{9,5},{13,1},{6,10},{2,14},... | collective-permute-start | bytes 393224 | tf_op jit(solution)/shard_map/ppermute | solution.py:119
  35.0 8.4 %collective-permute-start.13 = (f32[16,32,128]{2,1,0:T(8,128)S(1)}, f32[16,32,128]{2,1,0:T(8,128)S(1)}, u32[]{:S(2)}, u32[]{:S(2)}) collective-permute-start(f32[16,32,128]{2,1,0:T(8,128)S(1)} %add.50), channel_id=1, source_target_pairs={{0,2},{1,3},{2,0},{3,1},{4,6},{5,7},{6,4},{7,5},{8,10},{9,11},{10,... | collective-permute-start | bytes 786440 | tf_op jit(solution)/shard_map/ppermute | solution.py:515
  43.4 1.7 %collective-permute-start.14 = (f32[16,32,128]{2,1,0:T(8,128)S(1)}, f32[16,32,128]{2,1,0:T(8,128)S(1)}, u32[]{:S(2)}, u32[]{:S(2)}) collective-permute-start(f32[16,32,128]{2,1,0:T(8,128)S(1)} %add.52.refs_3_), channel_id=1, source_target_pairs={{0,1},{1,0},{2,3},{3,2},{4,5},{5,4},{6,7},{7,6},{8,9},{9,8},{10,11... | collective-permute-start | bytes 786440 | tf_op jit(solution)/shard_map/ppermute | solution.py:577
  44.6 2.0 %collective-permute-start.12 = (f32[16,32,128]{2,1,0:T(8,128)S(1)}, f32[16,32,128]{2,1,0:T(8,128)S(1)}, u32[]{:S(2)}, u32[]{:S(2)}) collective-permute-start(f32[16,32,128]{2,1,0:T(8,128)S(1)} %get-tuple-element.103), channel_id=1, source_target_pairs={{0,1},{1,0},{2,3},{3,2},{4,5},{5,4},{6,7},{7,6},{8,9},{9,8},{10,11... | collective-permute-start | bytes 786440 | tf_op jit(solution)/shard_map/ppermute | solution.py:581
  46.6 8.3 %collective-permute-start.15 = (f32[16,32,128]{2,1,0:T(8,128)S(1)}, f32[16,32,128]{2,1,0:T(8,128)S(1)}, u32[]{:S(2)}, u32[]{:S(2)}) collective-permute-start(f32[16,32,128]{2,1,0:T(8,128)S(1)} %add.53), channel_id=1, source_target_pairs={{0,2},{1,3},{2,0},{3,1},{4,6},{5,7},{6,4},{7,5},{8,10},{9,11},{10,... | collective-permute-start | bytes 786440 | tf_op jit(solution)/shard_map/ppermute | solution.py:515
  48.2 10.7 %collective-permute-start.17 = (f32[8,32,128]{2,1,0:T(8,128)S(1)}, f32[8,32,128]{2,1,0:T(8,128)S(1)}, u32[]{:S(2)}, u32[]{:S(2)}) collective-permute-start(f32[8,32,128]{2,1,0:T(8,128)S(1)} %get-tuple-element.111), channel_id=1, source_target_pairs={{0,8},{4,12},{8,0},{12,4},{1,9},{5,13},{9,1},{13,5},{2,10},{6,14},... | collective-permute-start | bytes 393224 | tf_op jit(solution)/shard_map/ppermute | solution.py:119
  50.4 12.0 %collective-permute-start.21 = (f32[8,32,128]{2,1,0:T(8,128)S(1)}, f32[8,32,128]{2,1,0:T(8,128)S(1)}, u32[]{:S(2)}, u32[]{:S(2)}) collective-permute-start(f32[8,32,128]{2,1,0:T(8,128)S(1)} %get-tuple-element.118), channel_id=1, source_target_pairs={{0,4},{8,12},{4,0},{12,8},{1,5},{9,13},{5,1},{13,9},{2,6},{10,14},... | collective-permute-start | bytes 393224 | tf_op jit(solution)/shard_map/ppermute | solution.py:119
  51.9 9.5 %collective-permute-start.22 = (f32[8,32,128]{2,1,0:T(8,128)S(1)}, f32[8,32,128]{2,1,0:T(8,128)S(1)}, u32[]{:S(2)}, u32[]{:S(2)}) collective-permute-start(f32[8,32,128]{2,1,0:T(8,128)S(1)} %get-tuple-element.119), channel_id=1, source_target_pairs={{4,8},{0,12},{8,4},{12,0},{5,9},{1,13},{9,5},{13,1},{6,10},{2,14},... | collective-permute-start | bytes 393224 | tf_op jit(solution)/shard_map/ppermute | solution.py:119
  55.0 4.8 %collective-permute-start.16 = (f32[16,32,128]{2,1,0:T(8,128)S(1)}, f32[16,32,128]{2,1,0:T(8,128)S(1)}, u32[]{:S(2)}, u32[]{:S(2)}) collective-permute-start(f32[16,32,128]{2,1,0:T(8,128)S(1)} %add.54.refs_3_), channel_id=1, source_target_pairs={{0,1},{1,0},{2,3},{3,2},{4,5},{5,4},{6,7},{7,6},{8,9},{9,8},{10,11... | collective-permute-start | bytes 786440 | tf_op jit(solution)/shard_map/ppermute | solution.py:585
  61.3 8.1 %collective-permute-start.20 = (f32[8,32,128]{2,1,0:T(8,128)S(1)}, f32[8,32,128]{2,1,0:T(8,128)S(1)}, u32[]{:S(2)}, u32[]{:S(2)}) collective-permute-start(f32[8,32,128]{2,1,0:T(8,128)S(1)} %get-tuple-element.116), channel_id=1, source_target_pairs={{0,4},{8,12},{4,0},{12,8},{1,5},{9,13},{5,1},{13,9},{2,6},{10,14},... | collective-permute-start | bytes 393224 | tf_op jit(solution)/shard_map/ppermute | solution.py:119
  63.5 12.4 %collective-permute-start.18 = (f32[8,32,128]{2,1,0:T(8,128)S(1)}, f32[8,32,128]{2,1,0:T(8,128)S(1)}, u32[]{:S(2)}, u32[]{:S(2)}) collective-permute-start(f32[8,32,128]{2,1,0:T(8,128)S(1)} %get-tuple-element.114), channel_id=1, source_target_pairs={{0,8},{4,12},{8,0},{12,4},{1,9},{5,13},{9,1},{13,5},{2,10},{6,14},... | collective-permute-start | bytes 393224 | tf_op jit(solution)/shard_map/ppermute | solution.py:119
  65.3 8.1 %collective-permute-start.19 = (f32[8,32,128]{2,1,0:T(8,128)S(1)}, f32[8,32,128]{2,1,0:T(8,128)S(1)}, u32[]{:S(2)}, u32[]{:S(2)}) collective-permute-start(f32[8,32,128]{2,1,0:T(8,128)S(1)} %get-tuple-element.115), channel_id=1, source_target_pairs={{4,8},{0,12},{8,4},{12,0},{5,9},{1,13},{9,5},{13,1},{6,10},{2,14},... | collective-permute-start | bytes 393224 | tf_op jit(solution)/shard_map/ppermute | solution.py:119
  67.6 2.7 %collective-permute-start.23 = (f32[16,32,128]{2,1,0:T(8,128)S(1)}, f32[16,32,128]{2,1,0:T(8,128)S(1)}, u32[]{:S(2)}, u32[]{:S(2)}) collective-permute-start(f32[16,32,128]{2,1,0:T(8,128)S(1)} %get-tuple-element.125), channel_id=1, source_target_pairs={{0,1},{1,0},{2,3},{3,2},{4,5},{5,4},{6,7},{7,6},{8,9},{9,8},{10,11... | collective-permute-start | bytes 786440 | tf_op jit(solution)/shard_map/ppermute | solution.py:591
  71.4 4.5 %collective-permute-start.24 = (f32[64,128]{1,0:T(8,128)S(1)}, f32[64,128]{1,0:T(8,128)S(1)}, u32[]{:S(2)}, u32[]{:S(2)}) collective-permute-start(f32[64,128]{1,0:T(8,128)S(1)} %cross.1), channel_id=1, source_target_pairs={{0,4},{4,0},{8,12},{12,8},{1,5},{5,1},{9,13},{13,9},{2,6},{6,2},{1... | collective-permute-start | bytes 98312 | tf_op jit(solution)/shard_map/ppermute | solution.py:140
  71.5 8.8 %collective-permute-start.26 = (f32[16,32,128]{2,1,0:T(8,128)S(1)}, f32[16,32,128]{2,1,0:T(8,128)S(1)}, u32[]{:S(2)}, u32[]{:S(2)}) collective-permute-start(f32[16,32,128]{2,1,0:T(8,128)S(1)} %add.55), channel_id=1, source_target_pairs={{0,2},{1,3},{2,0},{3,1},{4,6},{5,7},{6,4},{7,5},{8,10},{9,11},{10,... | collective-permute-start | bytes 786440 | tf_op jit(solution)/shard_map/ppermute | solution.py:515
  77.0 3.4 %collective-permute-start.25 = (f32[16,32,128]{2,1,0:T(8,128)S(1)}, f32[16,32,128]{2,1,0:T(8,128)S(1)}, u32[]{:S(2)}, u32[]{:S(2)}) collective-permute-start(f32[16,32,128]{2,1,0:T(8,128)S(1)} %get-tuple-element.131), channel_id=1, source_target_pairs={{0,1},{1,0},{2,3},{3,2},{4,5},{5,4},{6,7},{7,6},{8,9},{9,8},{10,11... | collective-permute-start | bytes 786440 | tf_op jit(solution)/shard_map/ppermute | solution.py:600
  80.3 9.5 %collective-permute-start.28 = (f32[16,32,128]{2,1,0:T(8,128)S(1)}, f32[16,32,128]{2,1,0:T(8,128)S(1)}, u32[]{:S(2)}, u32[]{:S(2)}) collective-permute-start(f32[16,32,128]{2,1,0:T(8,128)S(1)} %add.57.mine_ref), channel_id=1, source_target_pairs={{0,1},{1,0},{2,3},{3,2},{4,5},{5,4},{6,7},{7,6},{8,9},{9,8},{10,11... | collective-permute-start | bytes 786440 | tf_op jit(solution)/shard_map/ppermute | solution.py:602
  80.5 12.8 %collective-permute-start.27 = (f32[16,32,128]{2,1,0:T(8,128)S(1)}, f32[16,32,128]{2,1,0:T(8,128)S(1)}, u32[]{:S(2)}, u32[]{:S(2)}) collective-permute-start(f32[16,32,128]{2,1,0:T(8,128)S(1)} %add.58), channel_id=1, source_target_pairs={{0,2},{1,3},{2,0},{3,1},{4,6},{5,7},{6,4},{7,5},{8,10},{9,11},{10,... | collective-permute-start | bytes 786440 | tf_op jit(solution)/shard_map/ppermute | solution.py:515
  81.1 4.8 %collective-permute-start.29 = (f32[64,128]{1,0:T(8,128)S(1)}, f32[64,128]{1,0:T(8,128)S(1)}, u32[]{:S(2)}, u32[]{:S(2)}) collective-permute-start(f32[64,128]{1,0:T(8,128)S(1)} %add.56), channel_id=1, source_target_pairs={{0,8},{4,12},{8,0},{12,4},{1,9},{5,13},{9,1},{13,5},{2,10},{6,14},... | collective-permute-start | bytes 98312 | tf_op jit(solution)/shard_map/ppermute | solution.py:149
  97.0 6.0 %collective-permute-start.33 = (f32[72,128]{1,0:T(8,128)S(1)}, f32[72,128]{1,0:T(8,128)S(1)}, u32[]{:S(2)}, u32[]{:S(2)}) collective-permute-start(f32[72,128]{1,0:T(8,128)S(1)} %get-tuple-element.146), channel_id=1, source_target_pairs={{0,12},{4,8},{8,4},{12,0},{1,13},{5,9},{9,5},{13,1},{2,14},{6,10},... | collective-permute-start | bytes 110600 | tf_op jit(solution)/shard_map/ppermute | solution.py:161
  98.1 6.2 %collective-permute-start.32 = (f32[72,128]{1,0:T(8,128)S(1)}, f32[72,128]{1,0:T(8,128)S(1)}, u32[]{:S(2)}, u32[]{:S(2)}) collective-permute-start(f32[72,128]{1,0:T(8,128)S(1)} %get-tuple-element.146), channel_id=1, source_target_pairs={{0,8},{4,12},{8,0},{12,4},{1,9},{5,13},{9,1},{13,5},{2,10},{6,14},... | collective-permute-start | bytes 110600 | tf_op jit(solution)/shard_map/ppermute | solution.py:161
  100.1 4.4 %collective-permute-start.31 = (f32[72,128]{1,0:T(8,128)S(1)}, f32[72,128]{1,0:T(8,128)S(1)}, u32[]{:S(2)}, u32[]{:S(2)}) collective-permute-start(f32[72,128]{1,0:T(8,128)S(1)} %get-tuple-element.146), channel_id=1, source_target_pairs={{0,4},{4,0},{8,12},{12,8},{1,5},{5,1},{9,13},{13,9},{2,6},{6,2},{1... | collective-permute-start | bytes 110600 | tf_op jit(solution)/shard_map/ppermute | solution.py:161
  (6 other events, 31.0 us)

commit v14 on v13

--- a/solution.py
+++ b/solution.py
@@ -600,8 +600,8 @@
     core = lax.ppermute(give_b, "vec", swap)
     mine_a = across(mine_a, cross_gram)
     other_a = lax.ppermute(mine_a, "vec", swap)
-    mine_b = keep_b + after(core, mine_a)
-    cross_gram = end_sum(cross_gram, "res", mine_b)
+    cross_gram = end_sum(cross_gram, "res")
+    mine_b = keep_b + after(core, mine_a, cross_gram)
     cross1, lower1, coef, gain = call(
         second_body, [square, square, (2 * width, 3 * width), square], [VMEM] * 2, name="second"
     )(after(cross_gram, mine_b), start_inv)

time: 110 us -> 109 us (level)
  waiting for transfers between devices: 24.6 us -> 21.3 us
  starting transfers between devices: 39.8 us -> 41.7 us
    ppermute x4, waiting for transfers between devices: 4.25 us -> 1.8 us  [across(): got = lax.ppermute(mine, 'vec', [(i, i ^ step) for i in range(lanes)])]
    ppermute x2, starting transfers between devices: 1.46 us -> 3.37 us  [end_sum(): got = lax.ppermute(block, axis, [(i, i ^ step) for i in range(size)])]
    ppermute x2, waiting for transfers between devices: 5.97 us -> 4.45 us  [end_sum(): got = lax.ppermute(block, axis, [(i, i ^ step) for i in range(size)])]
  transfers between devices with their start and end apart: 34 -> 34, of which waited for: 15 -> 15; matrix products, arithmetic and copies ran while one was open for 1% -> 1% of each run, Pallas kernels for 31% -> 32%
where the time goes in v14:
time: 109 us
  Pallas kernels  43.4 us (40%)
  starting transfers between devices  41.7 us (38%)
  waiting for transfers between devices  21.3 us (20%)
    ppermute x15, starting transfers between devices, exchange(): lax.ppermute(block, axis, [(a, b) for a, b in pairs] + [(b, a) for a, b i...  27.2 us
    pallas_call x12, Pallas kernels, join(): call(body, [halfchunk] * 2 if last else [chunk], [SMEM] * (3 + size) + [V...  11.9 us
    ppermute x15, waiting for transfers between devices, exchange(): lax.ppermute(block, axis, [(a, b) for a, b in pairs] + [(b, a) for a, b i...  7.59 us
    pallas_call x3, Pallas kernels, own(): call(own_body, [chunk] * len(accs), [SMEM] * 2 + [VMEM] * (2 + len(accs))...  5.46 us
    ppermute x2, waiting for transfers between devices, end_sum(): got = lax.ppermute(block, axis, [(i, i ^ step) for i in range(size)])  4.45 us
    ppermute x3, starting transfers between devices, all_sum(): lax.ppermute(block, axis, [(i, i ^ m) for i in range(size)])  4.42 us
    ppermute x4, starting transfers between devices, across(): got = lax.ppermute(mine, 'vec', [(i, i ^ step) for i in range(lanes)])  4.3 us
    pallas_call x1, Pallas kernels, local(): call(second_body, [square, square, (2 * width, 3 * width), square], [VMEM...  3.94 us
  transfers between devices with their start and end apart: 34, of which 15 were waited for; matrix products, arithmetic and copies ran while one was open for 1% of the time, Pallas kernels for 32%

profile of v14, /device:TPU:0, one launch (start us, length us, event | category | flops | bytes accessed | tf_op | source)
XLA Modules:
  0.0 108.6 jit_solution(2735738650669128229)
XLA Ops:
  0.6 5.1 %collective-permute-start.2 = (s32[1,1,44]{2,1,0:T(1,128)}, s32[1,1,44]{2,1,0:T(1,128)S(1)}, u32[]{:S(2)}, u32[]{:S(2)}) collective-permute-start(s32[1,1,44]{2,1,0:T(1,128)} %cols_ref.5), channel_id=1, source_target_pairs={{4,8},{0,12},{8,4},{12,0},{5,9},{1,13},{9,5},{13,1},{6,10},{2,14},... | collective-permute-start | bytes 536 | tf_op jit(solution)/shard_map/ppermute | solution.py:119
  7.2 2.3 %prepare.1 = (f32[32,64,128]{2,1,0:T(8,128)S(1)}, bf16[44,2,128,128]{3,2,1,0:T(8,128)(2,1)S(1)}, f32[32,32,128]{2,1,0:T(8,128)S(1)}, f32[32,32,128]{2,1,0:T(8,128)S(1)}) custom-call(f32[32,64,128]{2,1,0:T(8,128)} %x_hbm.1, f32[32,128]{1,0:T(8,128)} %refs_5_.3, f32[1,1,44,128,128]{4,3,2,1,0:T(8,128)} %tiles_hbm.1), custom_call_target="tpu_custom_call" | custom-call | tf_op jit(solution)/shard_map/prepare/pallas_call | solution.py:539
  11.8 1.8 %collective-permute-start.5 = (f32[8,32,128]{2,1,0:T(8,128)S(1)}, f32[8,32,128]{2,1,0:T(8,128)S(1)}, u32[]{:S(2)}, u32[]{:S(2)}) collective-permute-start(f32[8,32,128]{2,1,0:T(8,128)S(1)} %get-tuple-element.81), channel_id=1, source_target_pairs={{0,4},{8,12},{4,0},{12,8},{1,5},{9,13},{5,1},{13,9},{2,6},{10,14},... | collective-permute-start | bytes 393224 | tf_op jit(solution)/shard_map/ppermute | solution.py:119
  14.6 1.6 %collective-permute-start.4 = (f32[8,32,128]{2,1,0:T(8,128)S(1)}, f32[8,32,128]{2,1,0:T(8,128)S(1)}, u32[]{:S(2)}, u32[]{:S(2)}) collective-permute-start(f32[8,32,128]{2,1,0:T(8,128)S(1)} %get-tuple-element.80), channel_id=1, source_target_pairs={{4,8},{0,12},{8,4},{12,0},{5,9},{1,13},{9,5},{13,1},{6,10},{2,14},... | collective-permute-start | bytes 393224 | tf_op jit(solution)/shard_map/ppermute | solution.py:119
  16.2 2.0 %own.3 = (f32[32,32,128]{2,1,0:T(8,128)S(1)}, f32[32,32,128]{2,1,0:T(8,128)S(1)}) custom-call(s32[1,1,44]{2,1,0:T(1,128)S(1)} %copy-done.1, s32[1,1,44]{2,1,0:T(1,128)S(1)} %copy-done.2, f32[32,64,128]{2,1,0:T(8,128)S(1)} %get-tuple-element.123.refs_3_.x_ref, ...), custom_call_target="tpu_custom_call", output_to_operand_aliasing={{0}: (4, {}), {1}: (5, {})} | custom-call | tf_op jit(solution)/shard_map/own/pallas_call | solution.py:530
  21.2 1.7 %collective-permute-done.4.refs_1_ = f32[8,32,128]{2,1,0:T(8,128)S(1)} collective-permute-done((f32[8,32,128]{2,1,0:T(8,128)S(1)}, f32[8,32,128]{2,1,0:T(8,128)S(1)}, u32[]{:S(2)}, u32[]{:S(2)}) %collective-permute-start.4) | collective-permute-done | bytes 131104 | tf_op jit(solution)/shard_map/ppermute | solution.py:119
  23.9 3.9 %collective-permute-start.9 = (f32[8,32,128]{2,1,0:T(8,128)S(1)}, f32[8,32,128]{2,1,0:T(8,128)S(1)}, u32[]{:S(2)}, u32[]{:S(2)}) collective-permute-start(f32[8,32,128]{2,1,0:T(8,128)S(1)} %get-tuple-element.95), channel_id=1, source_target_pairs={{0,4},{8,12},{4,0},{12,8},{1,5},{9,13},{5,1},{13,9},{2,6},{10,14},... | collective-permute-start | bytes 393224 | tf_op jit(solution)/shard_map/ppermute | solution.py:119
  29.0 2.6 %collective-permute-start.7 = (f32[8,32,128]{2,1,0:T(8,128)S(1)}, f32[8,32,128]{2,1,0:T(8,128)S(1)}, u32[]{:S(2)}, u32[]{:S(2)}) collective-permute-start(f32[8,32,128]{2,1,0:T(8,128)S(1)} %get-tuple-element.92), channel_id=1, source_target_pairs={{0,8},{4,12},{8,0},{12,4},{1,9},{5,13},{9,1},{13,5},{2,10},{6,14},... | collective-permute-start | bytes 393224 | tf_op jit(solution)/shard_map/ppermute | solution.py:119
  31.6 1.9 %collective-permute-start.8 = (f32[8,32,128]{2,1,0:T(8,128)S(1)}, f32[8,32,128]{2,1,0:T(8,128)S(1)}, u32[]{:S(2)}, u32[]{:S(2)}) collective-permute-start(f32[8,32,128]{2,1,0:T(8,128)S(1)} %get-tuple-element.94), channel_id=1, source_target_pairs={{4,8},{0,12},{8,4},{12,0},{5,9},{1,13},{9,5},{13,1},{6,10},{2,14},... | collective-permute-start | bytes 393224 | tf_op jit(solution)/shard_map/ppermute | solution.py:119
  35.0 1.6 %collective-permute-start.13 = (f32[16,32,128]{2,1,0:T(8,128)S(1)}, f32[16,32,128]{2,1,0:T(8,128)S(1)}, u32[]{:S(2)}, u32[]{:S(2)}) collective-permute-start(f32[16,32,128]{2,1,0:T(8,128)S(1)} %add.50), channel_id=1, source_target_pairs={{0,2},{1,3},{2,0},{3,1},{4,6},{5,7},{6,4},{7,5},{8,10},{9,11},{10,... | collective-permute-start | bytes 786440 | tf_op jit(solution)/shard_map/ppermute | solution.py:515
  36.5 2.5 %collective-permute-done.10 = f32[64,64]{1,0:T(8,128)S(1)} collective-permute-done((f32[64,64]{1,0:T(8,128)S(1)}, f32[64,64]{1,0:T(8,128)S(1)}, u32[]{:S(2)}, u32[]{:S(2)}) %collective-permute-start.10) | collective-permute-done | bytes 16416 | tf_op jit(solution)/shard_map/ppermute | solution.py:149
  39.0 3.0 %first.1.inverse_ref = f32[64,64]{1,0:T(8,128)S(1)} custom-call(f32[64,64]{1,0:T(8,128)S(1)} %add.51.gram_ref), custom_call_target="tpu_custom_call" | custom-call | tf_op jit(solution)/shard_map/first/pallas_call | solution.py:574
  46.6 1.6 %collective-permute-start.15 = (f32[16,32,128]{2,1,0:T(8,128)S(1)}, f32[16,32,128]{2,1,0:T(8,128)S(1)}, u32[]{:S(2)}, u32[]{:S(2)}) collective-permute-start(f32[16,32,128]{2,1,0:T(8,128)S(1)} %add.53), channel_id=1, source_target_pairs={{0,2},{1,3},{2,0},{3,1},{4,6},{5,7},{6,4},{7,5},{8,10},{9,11},{10,... | collective-permute-start | bytes 786440 | tf_op jit(solution)/shard_map/ppermute | solution.py:515
  48.6 1.7 %own.4.refs_3_ = f32[32,32,128]{2,1,0:T(8,128)S(1)} custom-call(s32[1,1,44]{2,1,0:T(1,128)S(1)} %copy-done.1, s32[1,1,44]{2,1,0:T(1,128)S(1)} %copy-done.2, f32[32,32,128]{2,1,0:T(8,128)S(1)} %get-tuple-element.105.x_ref.a_ref, bf16[44,2,128,128]{3,2,1,0:T(8,128)(2,1)S(1)} %get-tuple-element.77.refs_4_.split_ref.refs_2_.refs_6_, ...), custom_call_target="tpu_custom_call", output_to_operand_aliasing={{}: (4, {})} | custom-call | tf_op jit(solution)/shard_map/own/pallas_call | solution.py:530
  50.4 1.5 %collective-permute-start.21 = (f32[8,32,128]{2,1,0:T(8,128)S(1)}, f32[8,32,128]{2,1,0:T(8,128)S(1)}, u32[]{:S(2)}, u32[]{:S(2)}) collective-permute-start(f32[8,32,128]{2,1,0:T(8,128)S(1)} %get-tuple-element.117), channel_id=1, source_target_pairs={{0,4},{8,12},{4,0},{12,8},{1,5},{9,13},{5,1},{13,9},{2,6},{10,14},... | collective-permute-start | bytes 393224 | tf_op jit(solution)/shard_map/ppermute | solution.py:119
  51.9 2.5 %collective-permute-start.22 = (f32[8,32,128]{2,1,0:T(8,128)S(1)}, f32[8,32,128]{2,1,0:T(8,128)S(1)}, u32[]{:S(2)}, u32[]{:S(2)}) collective-permute-start(f32[8,32,128]{2,1,0:T(8,128)S(1)} %get-tuple-element.118), channel_id=1, source_target_pairs={{4,8},{0,12},{8,4},{12,0},{5,9},{1,13},{9,5},{13,1},{6,10},{2,14},... | collective-permute-start | bytes 393224 | tf_op jit(solution)/shard_map/ppermute | solution.py:119
  55.1 3.8 %collective-permute-done.17.refs_1_ = f32[8,32,128]{2,1,0:T(8,128)S(1)} collective-permute-done((f32[8,32,128]{2,1,0:T(8,128)S(1)}, f32[8,32,128]{2,1,0:T(8,128)S(1)}, u32[]{:S(2)}, u32[]{:S(2)}) %collective-permute-start.17) | collective-permute-done | bytes 131104 | tf_op jit(solution)/shard_map/ppermute | solution.py:119
  63.5 1.7 %collective-permute-start.18 = (f32[8,32,128]{2,1,0:T(8,128)S(1)}, f32[8,32,128]{2,1,0:T(8,128)S(1)}, u32[]{:S(2)}, u32[]{:S(2)}) collective-permute-start(f32[8,32,128]{2,1,0:T(8,128)S(1)} %get-tuple-element.113), channel_id=1, source_target_pairs={{0,8},{4,12},{8,0},{12,4},{1,9},{5,13},{9,1},{13,5},{2,10},{6,14},... | collective-permute-start | bytes 393224 | tf_op jit(solution)/shard_map/ppermute | solution.py:119
  65.3 2.4 %collective-permute-start.19 = (f32[8,32,128]{2,1,0:T(8,128)S(1)}, f32[8,32,128]{2,1,0:T(8,128)S(1)}, u32[]{:S(2)}, u32[]{:S(2)}) collective-permute-start(f32[8,32,128]{2,1,0:T(8,128)S(1)} %get-tuple-element.114), channel_id=1, source_target_pairs={{4,8},{0,12},{8,4},{12,0},{5,9},{1,13},{9,5},{13,1},{6,10},{2,14},... | collective-permute-start | bytes 393224 | tf_op jit(solution)/shard_map/ppermute | solution.py:119
  67.6 1.7 %own.5.refs_3_ = f32[32,32,128]{2,1,0:T(8,128)S(1)} custom-call(s32[1,1,44]{2,1,0:T(1,128)S(1)} %copy-done.1, s32[1,1,44]{2,1,0:T(1,128)S(1)} %copy-done.2, f32[32,32,128]{2,1,0:T(8,128)S(1)} %get-tuple-element.126.x_ref.b_ref, bf16[44,2,128,128]{3,2,1,0:T(8,128)(2,1)S(1)} %get-tuple-element.77.refs_4_.split_ref.refs_2_.refs_6_, ...), custom_call_target="tpu_custom_call", output_to_operand_aliasing={{}: (4, {})} | custom-call | tf_op jit(solution)/shard_map/own/pallas_call | solution.py:530
  74.4 1.6 %collective-permute-done.24 = f32[64,128]{1,0:T(8,128)S(1)} collective-permute-done((f32[64,128]{1,0:T(8,128)S(1)}, f32[64,128]{1,0:T(8,128)S(1)}, u32[]{:S(2)}, u32[]{:S(2)}) %collective-permute-start.24) | collective-permute-done | bytes 32800 | tf_op jit(solution)/shard_map/ppermute | solution.py:140
  77.1 3.2 %collective-permute-start.27 = (f32[64,128]{1,0:T(8,128)S(1)}, f32[64,128]{1,0:T(8,128)S(1)}, u32[]{:S(2)}, u32[]{:S(2)}) collective-permute-start(f32[64,128]{1,0:T(8,128)S(1)} %add.56), channel_id=1, source_target_pairs={{0,8},{4,12},{8,0},{12,4},{1,9},{5,13},{9,1},{13,5},{2,10},{6,14},... | collective-permute-start | bytes 98312 | tf_op jit(solution)/shard_map/ppermute | solution.py:149
  80.3 2.0 %collective-permute-done.27 = f32[64,128]{1,0:T(8,128)S(1)} collective-permute-done((f32[64,128]{1,0:T(8,128)S(1)}, f32[64,128]{1,0:T(8,128)S(1)}, u32[]{:S(2)}, u32[]{:S(2)}) %collective-permute-start.27) | collective-permute-done | bytes 32800 | tf_op jit(solution)/shard_map/ppermute | solution.py:149
  83.1 3.9 %second.1 = (f32[64,64]{1,0:T(8,128)S(1)}, f32[64,64]{1,0:T(8,128)S(1)}, f32[128,192]{1,0:T(8,128)S(1)}, f32[64,64]{1,0:T(8,128)S(1)}) custom-call(f32[64,128]{1,0:T(8,128)S(1)} %add.58.gram_ref, f32[64,64]{1,0:T(8,128)S(1)} %first.1.inverse_ref), custom_call_target="tpu_custom_call" | custom-call | tf_op jit(solution)/shard_map/second/pallas_call | solution.py:605
  87.0 1.7 %blend.3 = (f32[16,64,128]{2,1,0:T(8,128)S(1)}, f32[16,64,128]{2,1,0:T(8,128)S(1)}, f32[64,64]{1,0:T(8,128)S(1)}) custom-call(s32[4]{0:T(128)S(1)} %pad_add_fusion.place_ref, f32[32,64,128]{2,1,0:T(8,128)S(1)} %get-tuple-element.123.refs_3_.x_ref, f32[32,32,128]{2,1,0:T(8,128)S(1)} %get-tuple-element.105.x_ref.a_ref, ...), custom_call_target="tpu_custom_call" | custom-call | tf_op jit(solution)/shard_map/blend/pallas_call | solution.py:449
  88.7 1.7 %blend.2 = (f32[16,64,128]{2,1,0:T(8,128)S(1)}, f32[16,64,128]{2,1,0:T(8,128)S(1)}, f32[64,64]{1,0:T(8,128)S(1)}) custom-call(s32[4]{0:T(128)S(1)} %pad_add_fusion.place_ref, f32[32,64,128]{2,1,0:T(8,128)S(1)} %get-tuple-element.123.refs_3_.x_ref, f32[32,32,128]{2,1,0:T(8,128)S(1)} %get-tuple-element.105.x_ref.a_ref, ...), custom_call_target="tpu_custom_call" | custom-call | tf_op jit(solution)/shard_map/blend/pallas_call | solution.py:449
  92.9 2.0 %third.1 = (f32[32,64,128]{2,1,0:T(8,128)S(1)}, f32[72,128]{1,0:T(8,128)S(1)}) custom-call(s32[4]{0:T(128)S(1)} %pad_add_fusion.place_ref, f32[16,32,128]{2,1,0:T(8,128)S(1)} %add.60.mine_ref, f32[16,32,128]{2,1,0:T(8,128)S(1)} %collective-permute-done.30.other_ref, f32[64,64]{1,0:T(8,128)S(1)} %get-tuple-element.138.gain_ref, ...), custom_call_target="tpu_custom_call" | custom-call | tf_op jit(solution)/shard_map/third/pallas_call | solution.py:612
  94.9 2.3 %collective-permute-start.33 = (f32[72,128]{1,0:T(8,128)S(1)}, f32[72,128]{1,0:T(8,128)S(1)}, u32[]{:S(2)}, u32[]{:S(2)}) collective-permute-start(f32[72,128]{1,0:T(8,128)S(1)} %get-tuple-element.144), channel_id=1, source_target_pairs={{0,12},{4,8},{8,4},{12,0},{1,13},{5,9},{9,5},{13,1},{2,14},{6,10},... | collective-permute-start | bytes 110600 | tf_op jit(solution)/shard_map/ppermute | solution.py:161
  97.2 1.9 %collective-permute-start.32 = (f32[72,128]{1,0:T(8,128)S(1)}, f32[72,128]{1,0:T(8,128)S(1)}, u32[]{:S(2)}, u32[]{:S(2)}) collective-permute-start(f32[72,128]{1,0:T(8,128)S(1)} %get-tuple-element.144), channel_id=1, source_target_pairs={{0,8},{4,12},{8,0},{12,4},{1,9},{5,13},{9,1},{13,5},{2,10},{6,14},... | collective-permute-start | bytes 110600 | tf_op jit(solution)/shard_map/ppermute | solution.py:161
  100.7 1.6 %collective-permute-done.32 = f32[72,128]{1,0:T(8,128)S(1)} collective-permute-done((f32[72,128]{1,0:T(8,128)S(1)}, f32[72,128]{1,0:T(8,128)S(1)}, u32[]{:S(2)}, u32[]{:S(2)}) %collective-permute-start.32) | collective-permute-done | bytes 36896 | tf_op jit(solution)/shard_map/ppermute | solution.py:161
  103.1 3.7 %fourth.1 = (f32[64,64]{1,0:T(8,128)S(1)}, f32[64,64]{1,0:T(8,128)S(1)}, f32[64,128]{1,0:T(8,128)S(1)}) custom-call(f32[72,128]{1,0:T(8,128)S(1)} %add_add_fusion.gram_ref), custom_call_target="tpu_custom_call" | custom-call | tf_op jit(solution)/shard_map/fourth/pallas_call | solution.py:620
  106.8 1.9 %last.1 = (f32[32,64,128]{2,1,0:T(8,128)}, f32[4,64,64]{2,1,0:T(8,128)}) custom-call(f32[32,64,128]{2,1,0:T(8,128)S(1)} %get-tuple-element.143.w_ref, f32[16,64,128]{2,1,0:T(8,128)S(1)} %get-tuple-element.141.refs_2_.low_ref, f32[16,64,128]{2,1,0:T(8,128)S(1)} %get-tuple-element.142.refs_3_.high_ref, f32[64,128]{1,0:T(8,128)S(1)} %get-tuple-element.145.coef_ref, ...), custom_call_target="tpu_custom_call" | custom-call | tf_op jit(solution)/shard_map/last/pallas_call | solution.py:623
  (87 shorter events, 33.2 us)
Async XLA Ops:
  0.6 8.8 %collective-permute-start.2 = (s32[1,1,44]{2,1,0:T(1,128)}, s32[1,1,44]{2,1,0:T(1,128)S(1)}, u32[]{:S(2)}, u32[]{:S(2)}) collective-permute-start(s32[1,1,44]{2,1,0:T(1,128)} %cols_ref.5), channel_id=1, source_target_pairs={{4,8},{0,12},{8,4},{12,0},{5,9},{1,13},{9,5},{13,1},{6,10},{2,14},... | collective-permute-start | bytes 536 | tf_op jit(solution)/shard_map/ppermute | solution.py:119
  5.8 3.7 %collective-permute-start.1 = (s32[1,1,44]{2,1,0:T(1,128)}, s32[1,1,44]{2,1,0:T(1,128)S(1)}, u32[]{:S(2)}, u32[]{:S(2)}) collective-permute-start(s32[1,1,44]{2,1,0:T(1,128)} %cols_ref.5), channel_id=1, source_target_pairs={{0,4},{8,12},{4,0},{12,8},{1,5},{9,13},{5,1},{13,9},{2,6},{10,14},... | collective-permute-start | bytes 536 | tf_op jit(solution)/shard_map/ppermute | solution.py:119
  5.8 4.6 %collective-permute-start = (s32[1,1,44]{2,1,0:T(1,128)}, s32[1,1,44]{2,1,0:T(1,128)S(1)}, u32[]{:S(2)}, u32[]{:S(2)}) collective-permute-start(s32[1,1,44]{2,1,0:T(1,128)} %cols_ref.5), channel_id=1, source_target_pairs={{0,8},{4,12},{8,0},{12,4},{1,9},{5,13},{9,1},{13,5},{2,10},{6,14},... | collective-permute-start | bytes 536 | tf_op jit(solution)/shard_map/ppermute | solution.py:119
  11.8 6.5 %collective-permute-start.5 = (f32[8,32,128]{2,1,0:T(8,128)S(1)}, f32[8,32,128]{2,1,0:T(8,128)S(1)}, u32[]{:S(2)}, u32[]{:S(2)}) collective-permute-start(f32[8,32,128]{2,1,0:T(8,128)S(1)} %get-tuple-element.81), channel_id=1, source_target_pairs={{0,4},{8,12},{4,0},{12,8},{1,5},{9,13},{5,1},{13,9},{2,6},{10,14},... | collective-permute-start | bytes 393224 | tf_op jit(solution)/shard_map/ppermute | solution.py:119
  13.6 14.3 %collective-permute-start.3 = (f32[8,32,128]{2,1,0:T(8,128)S(1)}, f32[8,32,128]{2,1,0:T(8,128)S(1)}, u32[]{:S(2)}, u32[]{:S(2)}) collective-permute-start(f32[8,32,128]{2,1,0:T(8,128)S(1)} %get-tuple-element.79), channel_id=1, source_target_pairs={{0,8},{4,12},{8,0},{12,4},{1,9},{5,13},{9,1},{13,5},{2,10},{6,14},... | collective-permute-start | bytes 393224 | tf_op jit(solution)/shard_map/ppermute | solution.py:119
  14.6 8.3 %collective-permute-start.4 = (f32[8,32,128]{2,1,0:T(8,128)S(1)}, f32[8,32,128]{2,1,0:T(8,128)S(1)}, u32[]{:S(2)}, u32[]{:S(2)}) collective-permute-start(f32[8,32,128]{2,1,0:T(8,128)S(1)} %get-tuple-element.80), channel_id=1, source_target_pairs={{4,8},{0,12},{8,4},{12,0},{5,9},{1,13},{9,5},{13,1},{6,10},{2,14},... | collective-permute-start | bytes 393224 | tf_op jit(solution)/shard_map/ppermute | solution.py:119
  19.8 8.0 %collective-permute-start.6 = (f32[64,64]{1,0:T(8,128)S(1)}, f32[64,64]{1,0:T(8,128)S(1)}, u32[]{:S(2)}, u32[]{:S(2)}) collective-permute-start(f32[64,64]{1,0:T(8,128)S(1)} %gram.1), channel_id=1, source_target_pairs={{0,4},{4,0},{8,12},{12,8},{1,5},{5,1},{9,13},{13,9},{2,6},{6,2},{1... | collective-permute-start | bytes 49160 | tf_op jit(solution)/shard_map/ppermute | solution.py:140
  23.9 9.5 %collective-permute-start.9 = (f32[8,32,128]{2,1,0:T(8,128)S(1)}, f32[8,32,128]{2,1,0:T(8,128)S(1)}, u32[]{:S(2)}, u32[]{:S(2)}) collective-permute-start(f32[8,32,128]{2,1,0:T(8,128)S(1)} %get-tuple-element.95), channel_id=1, source_target_pairs={{0,4},{8,12},{4,0},{12,8},{1,5},{9,13},{5,1},{13,9},{2,6},{10,14},... | collective-permute-start | bytes 393224 | tf_op jit(solution)/shard_map/ppermute | solution.py:119
  27.8 11.2 %collective-permute-start.10 = (f32[64,64]{1,0:T(8,128)S(1)}, f32[64,64]{1,0:T(8,128)S(1)}, u32[]{:S(2)}, u32[]{:S(2)}) collective-permute-start(f32[64,64]{1,0:T(8,128)S(1)} %add.49), channel_id=1, source_target_pairs={{0,8},{4,12},{8,0},{12,4},{1,9},{5,13},{9,1},{13,5},{2,10},{6,14},... | collective-permute-start | bytes 49160 | tf_op jit(solution)/shard_map/ppermute | solution.py:149
  29.0 14.5 %collective-permute-start.7 = (f32[8,32,128]{2,1,0:T(8,128)S(1)}, f32[8,32,128]{2,1,0:T(8,128)S(1)}, u32[]{:S(2)}, u32[]{:S(2)}) collective-permute-start(f32[8,32,128]{2,1,0:T(8,128)S(1)} %get-tuple-element.92), channel_id=1, source_target_pairs={{0,8},{4,12},{8,0},{12,4},{1,9},{5,13},{9,1},{13,5},{2,10},{6,14},... | collective-permute-start | bytes 393224 | tf_op jit(solution)/shard_map/ppermute | solution.py:119
  31.6 10.5 %collective-permute-start.8 = (f32[8,32,128]{2,1,0:T(8,128)S(1)}, f32[8,32,128]{2,1,0:T(8,128)S(1)}, u32[]{:S(2)}, u32[]{:S(2)}) collective-permute-start(f32[8,32,128]{2,1,0:T(8,128)S(1)} %get-tuple-element.94), channel_id=1, source_target_pairs={{4,8},{0,12},{8,4},{12,0},{5,9},{1,13},{9,5},{13,1},{6,10},{2,14},... | collective-permute-start | bytes 393224 | tf_op jit(solution)/shard_map/ppermute | solution.py:119
  35.0 8.4 %collective-permute-start.13 = (f32[16,32,128]{2,1,0:T(8,128)S(1)}, f32[16,32,128]{2,1,0:T(8,128)S(1)}, u32[]{:S(2)}, u32[]{:S(2)}) collective-permute-start(f32[16,32,128]{2,1,0:T(8,128)S(1)} %add.50), channel_id=1, source_target_pairs={{0,2},{1,3},{2,0},{3,1},{4,6},{5,7},{6,4},{7,5},{8,10},{9,11},{10,... | collective-permute-start | bytes 786440 | tf_op jit(solution)/shard_map/ppermute | solution.py:515
  43.4 1.7 %collective-permute-start.14 = (f32[16,32,128]{2,1,0:T(8,128)S(1)}, f32[16,32,128]{2,1,0:T(8,128)S(1)}, u32[]{:S(2)}, u32[]{:S(2)}) collective-permute-start(f32[16,32,128]{2,1,0:T(8,128)S(1)} %add.52.refs_3_), channel_id=1, source_target_pairs={{0,1},{1,0},{2,3},{3,2},{4,5},{5,4},{6,7},{7,6},{8,9},{9,8},{10,11... | collective-permute-start | bytes 786440 | tf_op jit(solution)/shard_map/ppermute | solution.py:577
  44.6 2.0 %collective-permute-start.12 = (f32[16,32,128]{2,1,0:T(8,128)S(1)}, f32[16,32,128]{2,1,0:T(8,128)S(1)}, u32[]{:S(2)}, u32[]{:S(2)}) collective-permute-start(f32[16,32,128]{2,1,0:T(8,128)S(1)} %get-tuple-element.102), channel_id=1, source_target_pairs={{0,1},{1,0},{2,3},{3,2},{4,5},{5,4},{6,7},{7,6},{8,9},{9,8},{10,11... | collective-permute-start | bytes 786440 | tf_op jit(solution)/shard_map/ppermute | solution.py:581
  46.6 8.3 %collective-permute-start.15 = (f32[16,32,128]{2,1,0:T(8,128)S(1)}, f32[16,32,128]{2,1,0:T(8,128)S(1)}, u32[]{:S(2)}, u32[]{:S(2)}) collective-permute-start(f32[16,32,128]{2,1,0:T(8,128)S(1)} %add.53), channel_id=1, source_target_pairs={{0,2},{1,3},{2,0},{3,1},{4,6},{5,7},{6,4},{7,5},{8,10},{9,11},{10,... | collective-permute-start | bytes 786440 | tf_op jit(solution)/shard_map/ppermute | solution.py:515
  48.2 10.7 %collective-permute-start.17 = (f32[8,32,128]{2,1,0:T(8,128)S(1)}, f32[8,32,128]{2,1,0:T(8,128)S(1)}, u32[]{:S(2)}, u32[]{:S(2)}) collective-permute-start(f32[8,32,128]{2,1,0:T(8,128)S(1)} %get-tuple-element.110), channel_id=1, source_target_pairs={{0,8},{4,12},{8,0},{12,4},{1,9},{5,13},{9,1},{13,5},{2,10},{6,14},... | collective-permute-start | bytes 393224 | tf_op jit(solution)/shard_map/ppermute | solution.py:119
  50.4 12.0 %collective-permute-start.21 = (f32[8,32,128]{2,1,0:T(8,128)S(1)}, f32[8,32,128]{2,1,0:T(8,128)S(1)}, u32[]{:S(2)}, u32[]{:S(2)}) collective-permute-start(f32[8,32,128]{2,1,0:T(8,128)S(1)} %get-tuple-element.117), channel_id=1, source_target_pairs={{0,4},{8,12},{4,0},{12,8},{1,5},{9,13},{5,1},{13,9},{2,6},{10,14},... | collective-permute-start | bytes 393224 | tf_op jit(solution)/shard_map/ppermute | solution.py:119
  51.9 9.5 %collective-permute-start.22 = (f32[8,32,128]{2,1,0:T(8,128)S(1)}, f32[8,32,128]{2,1,0:T(8,128)S(1)}, u32[]{:S(2)}, u32[]{:S(2)}) collective-permute-start(f32[8,32,128]{2,1,0:T(8,128)S(1)} %get-tuple-element.118), channel_id=1, source_target_pairs={{4,8},{0,12},{8,4},{12,0},{5,9},{1,13},{9,5},{13,1},{6,10},{2,14},... | collective-permute-start | bytes 393224 | tf_op jit(solution)/shard_map/ppermute | solution.py:119
  55.0 4.8 %collective-permute-start.16 = (f32[16,32,128]{2,1,0:T(8,128)S(1)}, f32[16,32,128]{2,1,0:T(8,128)S(1)}, u32[]{:S(2)}, u32[]{:S(2)}) collective-permute-start(f32[16,32,128]{2,1,0:T(8,128)S(1)} %add.54.refs_3_), channel_id=1, source_target_pairs={{0,1},{1,0},{2,3},{3,2},{4,5},{5,4},{6,7},{7,6},{8,9},{9,8},{10,11... | collective-permute-start | bytes 786440 | tf_op jit(solution)/shard_map/ppermute | solution.py:585
  61.3 8.1 %collective-permute-start.20 = (f32[8,32,128]{2,1,0:T(8,128)S(1)}, f32[8,32,128]{2,1,0:T(8,128)S(1)}, u32[]{:S(2)}, u32[]{:S(2)}) collective-permute-start(f32[8,32,128]{2,1,0:T(8,128)S(1)} %get-tuple-element.115), channel_id=1, source_target_pairs={{0,4},{8,12},{4,0},{12,8},{1,5},{9,13},{5,1},{13,9},{2,6},{10,14},... | collective-permute-start | bytes 393224 | tf_op jit(solution)/shard_map/ppermute | solution.py:119
  63.5 12.4 %collective-permute-start.18 = (f32[8,32,128]{2,1,0:T(8,128)S(1)}, f32[8,32,128]{2,1,0:T(8,128)S(1)}, u32[]{:S(2)}, u32[]{:S(2)}) collective-permute-start(f32[8,32,128]{2,1,0:T(8,128)S(1)} %get-tuple-element.113), channel_id=1, source_target_pairs={{0,8},{4,12},{8,0},{12,4},{1,9},{5,13},{9,1},{13,5},{2,10},{6,14},... | collective-permute-start | bytes 393224 | tf_op jit(solution)/shard_map/ppermute | solution.py:119
  65.3 8.1 %collective-permute-start.19 = (f32[8,32,128]{2,1,0:T(8,128)S(1)}, f32[8,32,128]{2,1,0:T(8,128)S(1)}, u32[]{:S(2)}, u32[]{:S(2)}) collective-permute-start(f32[8,32,128]{2,1,0:T(8,128)S(1)} %get-tuple-element.114), channel_id=1, source_target_pairs={{4,8},{0,12},{8,4},{12,0},{5,9},{1,13},{9,5},{13,1},{6,10},{2,14},... | collective-permute-start | bytes 393224 | tf_op jit(solution)/shard_map/ppermute | solution.py:119
  67.6 2.7 %collective-permute-start.23 = (f32[16,32,128]{2,1,0:T(8,128)S(1)}, f32[16,32,128]{2,1,0:T(8,128)S(1)}, u32[]{:S(2)}, u32[]{:S(2)}) collective-permute-start(f32[16,32,128]{2,1,0:T(8,128)S(1)} %get-tuple-element.124), channel_id=1, source_target_pairs={{0,1},{1,0},{2,3},{3,2},{4,5},{5,4},{6,7},{7,6},{8,9},{9,8},{10,11... | collective-permute-start | bytes 786440 | tf_op jit(solution)/shard_map/ppermute | solution.py:591
  71.4 4.5 %collective-permute-start.24 = (f32[64,128]{1,0:T(8,128)S(1)}, f32[64,128]{1,0:T(8,128)S(1)}, u32[]{:S(2)}, u32[]{:S(2)}) collective-permute-start(f32[64,128]{1,0:T(8,128)S(1)} %cross.1), channel_id=1, source_target_pairs={{0,4},{4,0},{8,12},{12,8},{1,5},{5,1},{9,13},{13,9},{2,6},{6,2},{1... | collective-permute-start | bytes 98312 | tf_op jit(solution)/shard_map/ppermute | solution.py:140
  71.5 10.8 %collective-permute-start.26 = (f32[16,32,128]{2,1,0:T(8,128)S(1)}, f32[16,32,128]{2,1,0:T(8,128)S(1)}, u32[]{:S(2)}, u32[]{:S(2)}) collective-permute-start(f32[16,32,128]{2,1,0:T(8,128)S(1)} %add.55), channel_id=1, source_target_pairs={{0,2},{1,3},{2,0},{3,1},{4,6},{5,7},{6,4},{7,5},{8,10},{9,11},{10,... | collective-permute-start | bytes 786440 | tf_op jit(solution)/shard_map/ppermute | solution.py:515
  77.0 5.4 %collective-permute-start.25 = (f32[16,32,128]{2,1,0:T(8,128)S(1)}, f32[16,32,128]{2,1,0:T(8,128)S(1)}, u32[]{:S(2)}, u32[]{:S(2)}) collective-permute-start(f32[16,32,128]{2,1,0:T(8,128)S(1)} %get-tuple-element.130), channel_id=1, source_target_pairs={{0,1},{1,0},{2,3},{3,2},{4,5},{5,4},{6,7},{7,6},{8,9},{9,8},{10,11... | collective-permute-start | bytes 786440 | tf_op jit(solution)/shard_map/ppermute | solution.py:600
  77.1 5.2 %collective-permute-start.27 = (f32[64,128]{1,0:T(8,128)S(1)}, f32[64,128]{1,0:T(8,128)S(1)}, u32[]{:S(2)}, u32[]{:S(2)}) collective-permute-start(f32[64,128]{1,0:T(8,128)S(1)} %add.56), channel_id=1, source_target_pairs={{0,8},{4,12},{8,0},{12,4},{1,9},{5,13},{9,1},{13,5},{2,10},{6,14},... | collective-permute-start | bytes 98312 | tf_op jit(solution)/shard_map/ppermute | solution.py:149
  82.3 4.7 %collective-permute-start.29 = (f32[16,32,128]{2,1,0:T(8,128)S(1)}, f32[16,32,128]{2,1,0:T(8,128)S(1)}, u32[]{:S(2)}, u32[]{:S(2)}) collective-permute-start(f32[16,32,128]{2,1,0:T(8,128)S(1)} %add.57.mine_ref), channel_id=1, source_target_pairs={{0,1},{1,0},{2,3},{3,2},{4,5},{5,4},{6,7},{7,6},{8,9},{9,8},{10,11... | collective-permute-start | bytes 786440 | tf_op jit(solution)/shard_map/ppermute | solution.py:602
  82.5 8.8 %collective-permute-start.28 = (f32[16,32,128]{2,1,0:T(8,128)S(1)}, f32[16,32,128]{2,1,0:T(8,128)S(1)}, u32[]{:S(2)}, u32[]{:S(2)}) collective-permute-start(f32[16,32,128]{2,1,0:T(8,128)S(1)} %add.59), channel_id=1, source_target_pairs={{0,2},{1,3},{2,0},{3,1},{4,6},{5,7},{6,4},{7,5},{8,10},{9,11},{10,... | collective-permute-start | bytes 786440 | tf_op jit(solution)/shard_map/ppermute | solution.py:515
  94.9 5.8 %collective-permute-start.33 = (f32[72,128]{1,0:T(8,128)S(1)}, f32[72,128]{1,0:T(8,128)S(1)}, u32[]{:S(2)}, u32[]{:S(2)}) collective-permute-start(f32[72,128]{1,0:T(8,128)S(1)} %get-tuple-element.144), channel_id=1, source_target_pairs={{0,12},{4,8},{8,4},{12,0},{1,13},{5,9},{9,5},{13,1},{2,14},{6,10},... | collective-permute-start | bytes 110600 | tf_op jit(solution)/shard_map/ppermute | solution.py:161
  97.2 5.1 %collective-permute-start.32 = (f32[72,128]{1,0:T(8,128)S(1)}, f32[72,128]{1,0:T(8,128)S(1)}, u32[]{:S(2)}, u32[]{:S(2)}) collective-permute-start(f32[72,128]{1,0:T(8,128)S(1)} %get-tuple-element.144), channel_id=1, source_target_pairs={{0,8},{4,12},{8,0},{12,4},{1,9},{5,13},{9,1},{13,5},{2,10},{6,14},... | collective-permute-start | bytes 110600 | tf_op jit(solution)/shard_map/ppermute | solution.py:161
  99.1 4.0 %collective-permute-start.31 = (f32[72,128]{1,0:T(8,128)S(1)}, f32[72,128]{1,0:T(8,128)S(1)}, u32[]{:S(2)}, u32[]{:S(2)}) collective-permute-start(f32[72,128]{1,0:T(8,128)S(1)} %get-tuple-element.144), channel_id=1, source_target_pairs={{0,4},{4,0},{8,12},{12,8},{1,5},{5,1},{9,13},{13,9},{2,6},{6,2},{1... | collective-permute-start | bytes 110600 | tf_op jit(solution)/shard_map/ppermute | solution.py:161
  (6 other events, 31.0 us)

commit v15 on v14

--- a/solution.py
+++ b/solution.py
@@ -176,39 +176,38 @@
     work = jnp.concatenate([gram, (row_id == col_id).astype(F32)], axis=1)
     blocks = [work[8 * b : 8 * b + 8] for b in range(size // 8)]
     sub = lax.broadcasted_iota(jnp.int32, tile, 0)
-    for j in range(0, size, 4):
-        b, s = divmod(j, 8)
-        later = range(b + s // 4, size // 8)
-        line = [jnp.broadcast_to(blocks[b][s + k : s + k + 1], tile) for k in range(4)]
-        cols = {
-            o: [jnp.broadcast_to(blocks[o][:, j + k : j + k + 1], tile) for k in range(4)]
-            for o in range(b, size // 8)
+
+    def column(block, j):
+        return jnp.broadcast_to(block[:, j : j + 1], tile)
+
+    for b in range(size // 8):
+        line = [jnp.broadcast_to(blocks[b][k : k + 1], tile) for k in range(8)]
+        cols = [column(blocks[b], 8 * b + k) for k in range(8)]
+        entry = {
+            (k, l): jnp.broadcast_to(cols[l][k : k + 1], tile) for k in range(8) for l in range(k, 8)
         }
-        entry = {
-            (k, l): jnp.broadcast_to(cols[b][l][s + k : s + k + 1], tile)
-            for k in range(4)
-            for l in range(k, 4)
-        }
-        scaled = []
-        for k in range(4):
+        ratio = {}
+        solved = []
+        for k in range(8):
             inverse = 1.0 / entry[k, k]
-            for l in range(k + 1, 4):
-                ratio = entry[k, l] * inverse
-                for p in range(l, 4):
-                    entry[l, p] = entry[l, p] - ratio * entry[k, p]
-                line[l] = line[l] - ratio * line[k]
-                for o in later:
-                    cols[o][l] = cols[o][l] - ratio * cols[o][k]
-            scaled.append(inverse * line[k])
-        for o in range(b, size // 8):
-            new = blocks[o]
-            if o in later:
-                new = new - ((cols[o][0] * scaled[0] + cols[o][1] * scaled[1]) + (cols[o][2] * scaled[2] + cols[o][3] * scaled[3]))
-            if o == b:
-                new = jnp.where(sub > s + 3, new, blocks[o])
-                for k in range(1, 4):
-                    new = jnp.where(sub == s + k, line[k], new)
-            blocks[o] = new
+            for l in range(k + 1, 8):
+                ratio[k, l] = entry[k, l] * inverse
+                for p in range(l, 8):
+                    entry[l, p] = entry[l, p] - ratio[k, l] * entry[k, p]
+                line[l] = line[l] - ratio[k, l] * line[k]
+            solved.append(inverse * line[k])
+        for l in reversed(range(1, 8)):
+            for k in range(l):
+                solved[k] = solved[k] - ratio[k, l] * solved[l]
+        for o in range(b + 1, size // 8):
+            terms = [column(blocks[o], 8 * b + k) * solved[k] for k in range(8)]
+            while len(terms) > 1:
+                terms = [terms[n] + terms[n + 1] for n in range(0, len(terms), 2)]
+            blocks[o] = blocks[o] - terms[0]
+        new = line[0]
+        for k in range(1, 8):
+            new = jnp.where(sub == k, line[k], new)
+        blocks[b] = new
     work = jnp.concatenate(blocks, axis=0)
     pivots = jnp.sum(jnp.where(row_id == col_id, work[:, :size], 0.0), axis=1, keepdims=True)
     work = work / jnp.sqrt(pivots)

time: 109 us -> 108 us (level)
  Pallas kernels: 43.4 us -> 41.8 us
  waiting for transfers between devices: 21.3 us -> 22.4 us
    ppermute x4, waiting for transfers between devices: 1.8 us -> 2.92 us  [across(): got = lax.ppermute(mine, 'vec', [(i, i ^ step) for i in range(lanes)])]
  transfers between devices with their start and end apart: 34 -> 34, of which waited for: 15 -> 15; matrix products, arithmetic and copies ran while one was open for 1% -> 1% of each run, Pallas kernels for 32% -> 31%
where the time goes in v15:
time: 108 us
  Pallas kernels  41.8 us (39%)
  starting transfers between devices  41.7 us (39%)
  waiting for transfers between devices  22.4 us (21%)
    ppermute x15, starting transfers between devices, exchange(): lax.ppermute(block, axis, [(a, b) for a, b in pairs] + [(b, a) for a, b i...  27.2 us
    pallas_call x12, Pallas kernels, join(): call(body, [halfchunk] * 2 if last else [chunk], [SMEM] * (3 + size) + [V...  11.9 us
    ppermute x15, waiting for transfers between devices, exchange(): lax.ppermute(block, axis, [(a, b) for a, b in pairs] + [(b, a) for a, b i...  7.57 us
    pallas_call x3, Pallas kernels, own(): call(own_body, [chunk] * len(accs), [SMEM] * 2 + [VMEM] * (2 + len(accs))...  5.46 us
    ppermute x2, waiting for transfers between devices, end_sum(): got = lax.ppermute(block, axis, [(i, i ^ step) for i in range(size)])  4.45 us
    ppermute x3, starting transfers between devices, all_sum(): lax.ppermute(block, axis, [(i, i ^ m) for i in range(size)])  4.42 us
    ppermute x4, starting transfers between devices, across(): got = lax.ppermute(mine, 'vec', [(i, i ^ step) for i in range(lanes)])  4.32 us
    ppermute x3, waiting for transfers between devices, all_sum(): lax.ppermute(block, axis, [(i, i ^ m) for i in range(size)])  3.77 us
  transfers between devices with their start and end apart: 34, of which 15 were waited for; matrix products, arithmetic and copies ran while one was open for 1% of the time, Pallas kernels for 31%

profile of v15, /device:TPU:0, one launch (start us, length us, event | category | flops | bytes accessed | tf_op | source)
XLA Modules:
  0.0 108.1 jit_solution(4063515134908709512)
XLA Ops:
  0.6 5.1 %collective-permute-start.2 = (s32[1,1,44]{2,1,0:T(1,128)}, s32[1,1,44]{2,1,0:T(1,128)S(1)}, u32[]{:S(2)}, u32[]{:S(2)}) collective-permute-start(s32[1,1,44]{2,1,0:T(1,128)} %cols_ref.5), channel_id=1, source_target_pairs={{4,8},{0,12},{8,4},{12,0},{5,9},{1,13},{9,5},{13,1},{6,10},{2,14},... | collective-permute-start | bytes 536 | tf_op jit(solution)/shard_map/ppermute | solution.py:119
  7.2 2.3 %prepare.1 = (f32[32,64,128]{2,1,0:T(8,128)S(1)}, bf16[44,2,128,128]{3,2,1,0:T(8,128)(2,1)S(1)}, f32[32,32,128]{2,1,0:T(8,128)S(1)}, f32[32,32,128]{2,1,0:T(8,128)S(1)}) custom-call(f32[32,64,128]{2,1,0:T(8,128)} %x_hbm.1, f32[32,128]{1,0:T(8,128)} %refs_5_.3, f32[1,1,44,128,128]{4,3,2,1,0:T(8,128)} %tiles_hbm.1), custom_call_target="tpu_custom_call" | custom-call | tf_op jit(solution)/shard_map/prepare/pallas_call | solution.py:538
  11.8 1.8 %collective-permute-start.5 = (f32[8,32,128]{2,1,0:T(8,128)S(1)}, f32[8,32,128]{2,1,0:T(8,128)S(1)}, u32[]{:S(2)}, u32[]{:S(2)}) collective-permute-start(f32[8,32,128]{2,1,0:T(8,128)S(1)} %get-tuple-element.81), channel_id=1, source_target_pairs={{0,4},{8,12},{4,0},{12,8},{1,5},{9,13},{5,1},{13,9},{2,6},{10,14},... | collective-permute-start | bytes 393224 | tf_op jit(solution)/shard_map/ppermute | solution.py:119
  14.6 1.6 %collective-permute-start.4 = (f32[8,32,128]{2,1,0:T(8,128)S(1)}, f32[8,32,128]{2,1,0:T(8,128)S(1)}, u32[]{:S(2)}, u32[]{:S(2)}) collective-permute-start(f32[8,32,128]{2,1,0:T(8,128)S(1)} %get-tuple-element.80), channel_id=1, source_target_pairs={{4,8},{0,12},{8,4},{12,0},{5,9},{1,13},{9,5},{13,1},{6,10},{2,14},... | collective-permute-start | bytes 393224 | tf_op jit(solution)/shard_map/ppermute | solution.py:119
  16.2 2.0 %own.3 = (f32[32,32,128]{2,1,0:T(8,128)S(1)}, f32[32,32,128]{2,1,0:T(8,128)S(1)}) custom-call(s32[1,1,44]{2,1,0:T(1,128)S(1)} %copy-done.1, s32[1,1,44]{2,1,0:T(1,128)S(1)} %copy-done.2, f32[32,64,128]{2,1,0:T(8,128)S(1)} %get-tuple-element.123.refs_3_.x_ref, ...), custom_call_target="tpu_custom_call", output_to_operand_aliasing={{0}: (4, {}), {1}: (5, {})} | custom-call | tf_op jit(solution)/shard_map/own/pallas_call | solution.py:529
  21.2 1.7 %collective-permute-done.4.refs_1_ = f32[8,32,128]{2,1,0:T(8,128)S(1)} collective-permute-done((f32[8,32,128]{2,1,0:T(8,128)S(1)}, f32[8,32,128]{2,1,0:T(8,128)S(1)}, u32[]{:S(2)}, u32[]{:S(2)}) %collective-permute-start.4) | collective-permute-done | bytes 131104 | tf_op jit(solution)/shard_map/ppermute | solution.py:119
  23.9 3.9 %collective-permute-start.9 = (f32[8,32,128]{2,1,0:T(8,128)S(1)}, f32[8,32,128]{2,1,0:T(8,128)S(1)}, u32[]{:S(2)}, u32[]{:S(2)}) collective-permute-start(f32[8,32,128]{2,1,0:T(8,128)S(1)} %get-tuple-element.95), channel_id=1, source_target_pairs={{0,4},{8,12},{4,0},{12,8},{1,5},{9,13},{5,1},{13,9},{2,6},{10,14},... | collective-permute-start | bytes 393224 | tf_op jit(solution)/shard_map/ppermute | solution.py:119
  29.0 2.6 %collective-permute-start.7 = (f32[8,32,128]{2,1,0:T(8,128)S(1)}, f32[8,32,128]{2,1,0:T(8,128)S(1)}, u32[]{:S(2)}, u32[]{:S(2)}) collective-permute-start(f32[8,32,128]{2,1,0:T(8,128)S(1)} %get-tuple-element.92), channel_id=1, source_target_pairs={{0,8},{4,12},{8,0},{12,4},{1,9},{5,13},{9,1},{13,5},{2,10},{6,14},... | collective-permute-start | bytes 393224 | tf_op jit(solution)/shard_map/ppermute | solution.py:119
  31.6 1.9 %collective-permute-start.8 = (f32[8,32,128]{2,1,0:T(8,128)S(1)}, f32[8,32,128]{2,1,0:T(8,128)S(1)}, u32[]{:S(2)}, u32[]{:S(2)}) collective-permute-start(f32[8,32,128]{2,1,0:T(8,128)S(1)} %get-tuple-element.94), channel_id=1, source_target_pairs={{4,8},{0,12},{8,4},{12,0},{5,9},{1,13},{9,5},{13,1},{6,10},{2,14},... | collective-permute-start | bytes 393224 | tf_op jit(solution)/shard_map/ppermute | solution.py:119
  35.0 1.6 %collective-permute-start.13 = (f32[16,32,128]{2,1,0:T(8,128)S(1)}, f32[16,32,128]{2,1,0:T(8,128)S(1)}, u32[]{:S(2)}, u32[]{:S(2)}) collective-permute-start(f32[16,32,128]{2,1,0:T(8,128)S(1)} %add.50), channel_id=1, source_target_pairs={{0,2},{1,3},{2,0},{3,1},{4,6},{5,7},{6,4},{7,5},{8,10},{9,11},{10,... | collective-permute-start | bytes 786440 | tf_op jit(solution)/shard_map/ppermute | solution.py:514
  36.5 2.5 %collective-permute-done.10 = f32[64,64]{1,0:T(8,128)S(1)} collective-permute-done((f32[64,64]{1,0:T(8,128)S(1)}, f32[64,64]{1,0:T(8,128)S(1)}, u32[]{:S(2)}, u32[]{:S(2)}) %collective-permute-start.10) | collective-permute-done | bytes 16416 | tf_op jit(solution)/shard_map/ppermute | solution.py:149
  39.0 2.4 %first.1.inverse_ref = f32[64,64]{1,0:T(8,128)S(1)} custom-call(f32[64,64]{1,0:T(8,128)S(1)} %add.51.gram_ref), custom_call_target="tpu_custom_call" | custom-call | tf_op jit(solution)/shard_map/first/pallas_call | solution.py:573
  46.6 1.6 %collective-permute-start.15 = (f32[16,32,128]{2,1,0:T(8,128)S(1)}, f32[16,32,128]{2,1,0:T(8,128)S(1)}, u32[]{:S(2)}, u32[]{:S(2)}) collective-permute-start(f32[16,32,128]{2,1,0:T(8,128)S(1)} %add.53), channel_id=1, source_target_pairs={{0,2},{1,3},{2,0},{3,1},{4,6},{5,7},{6,4},{7,5},{8,10},{9,11},{10,... | collective-permute-start | bytes 786440 | tf_op jit(solution)/shard_map/ppermute | solution.py:514
  48.6 1.7 %own.4.refs_3_ = f32[32,32,128]{2,1,0:T(8,128)S(1)} custom-call(s32[1,1,44]{2,1,0:T(1,128)S(1)} %copy-done.1, s32[1,1,44]{2,1,0:T(1,128)S(1)} %copy-done.2, f32[32,32,128]{2,1,0:T(8,128)S(1)} %get-tuple-element.105.x_ref.a_ref, bf16[44,2,128,128]{3,2,1,0:T(8,128)(2,1)S(1)} %get-tuple-element.77.refs_4_.split_ref.refs_2_.refs_6_, ...), custom_call_target="tpu_custom_call", output_to_operand_aliasing={{}: (4, {})} | custom-call | tf_op jit(solution)/shard_map/own/pallas_call | solution.py:529
  50.4 1.5 %collective-permute-start.21 = (f32[8,32,128]{2,1,0:T(8,128)S(1)}, f32[8,32,128]{2,1,0:T(8,128)S(1)}, u32[]{:S(2)}, u32[]{:S(2)}) collective-permute-start(f32[8,32,128]{2,1,0:T(8,128)S(1)} %get-tuple-element.117), channel_id=1, source_target_pairs={{0,4},{8,12},{4,0},{12,8},{1,5},{9,13},{5,1},{13,9},{2,6},{10,14},... | collective-permute-start | bytes 393224 | tf_op jit(solution)/shard_map/ppermute | solution.py:119
  51.9 2.5 %collective-permute-start.22 = (f32[8,32,128]{2,1,0:T(8,128)S(1)}, f32[8,32,128]{2,1,0:T(8,128)S(1)}, u32[]{:S(2)}, u32[]{:S(2)}) collective-permute-start(f32[8,32,128]{2,1,0:T(8,128)S(1)} %get-tuple-element.118), channel_id=1, source_target_pairs={{4,8},{0,12},{8,4},{12,0},{5,9},{1,13},{9,5},{13,1},{6,10},{2,14},... | collective-permute-start | bytes 393224 | tf_op jit(solution)/shard_map/ppermute | solution.py:119
  55.1 3.8 %collective-permute-done.17.refs_1_ = f32[8,32,128]{2,1,0:T(8,128)S(1)} collective-permute-done((f32[8,32,128]{2,1,0:T(8,128)S(1)}, f32[8,32,128]{2,1,0:T(8,128)S(1)}, u32[]{:S(2)}, u32[]{:S(2)}) %collective-permute-start.17) | collective-permute-done | bytes 131104 | tf_op jit(solution)/shard_map/ppermute | solution.py:119
  63.5 1.7 %collective-permute-start.18 = (f32[8,32,128]{2,1,0:T(8,128)S(1)}, f32[8,32,128]{2,1,0:T(8,128)S(1)}, u32[]{:S(2)}, u32[]{:S(2)}) collective-permute-start(f32[8,32,128]{2,1,0:T(8,128)S(1)} %get-tuple-element.113), channel_id=1, source_target_pairs={{0,8},{4,12},{8,0},{12,4},{1,9},{5,13},{9,1},{13,5},{2,10},{6,14},... | collective-permute-start | bytes 393224 | tf_op jit(solution)/shard_map/ppermute | solution.py:119
  65.3 2.4 %collective-permute-start.19 = (f32[8,32,128]{2,1,0:T(8,128)S(1)}, f32[8,32,128]{2,1,0:T(8,128)S(1)}, u32[]{:S(2)}, u32[]{:S(2)}) collective-permute-start(f32[8,32,128]{2,1,0:T(8,128)S(1)} %get-tuple-element.114), channel_id=1, source_target_pairs={{4,8},{0,12},{8,4},{12,0},{5,9},{1,13},{9,5},{13,1},{6,10},{2,14},... | collective-permute-start | bytes 393224 | tf_op jit(solution)/shard_map/ppermute | solution.py:119
  67.6 1.7 %own.5.refs_3_ = f32[32,32,128]{2,1,0:T(8,128)S(1)} custom-call(s32[1,1,44]{2,1,0:T(1,128)S(1)} %copy-done.1, s32[1,1,44]{2,1,0:T(1,128)S(1)} %copy-done.2, f32[32,32,128]{2,1,0:T(8,128)S(1)} %get-tuple-element.126.x_ref.b_ref, bf16[44,2,128,128]{3,2,1,0:T(8,128)(2,1)S(1)} %get-tuple-element.77.refs_4_.split_ref.refs_2_.refs_6_, ...), custom_call_target="tpu_custom_call", output_to_operand_aliasing={{}: (4, {})} | custom-call | tf_op jit(solution)/shard_map/own/pallas_call | solution.py:529
  74.3 1.6 %collective-permute-done.24 = f32[64,128]{1,0:T(8,128)S(1)} collective-permute-done((f32[64,128]{1,0:T(8,128)S(1)}, f32[64,128]{1,0:T(8,128)S(1)}, u32[]{:S(2)}, u32[]{:S(2)}) %collective-permute-start.24) | collective-permute-done | bytes 32800 | tf_op jit(solution)/shard_map/ppermute | solution.py:140
  77.1 3.2 %collective-permute-start.27 = (f32[64,128]{1,0:T(8,128)S(1)}, f32[64,128]{1,0:T(8,128)S(1)}, u32[]{:S(2)}, u32[]{:S(2)}) collective-permute-start(f32[64,128]{1,0:T(8,128)S(1)} %add.56), channel_id=1, source_target_pairs={{0,8},{4,12},{8,0},{12,4},{1,9},{5,13},{9,1},{13,5},{2,10},{6,14},... | collective-permute-start | bytes 98312 | tf_op jit(solution)/shard_map/ppermute | solution.py:149
  80.3 2.0 %collective-permute-done.27 = f32[64,128]{1,0:T(8,128)S(1)} collective-permute-done((f32[64,128]{1,0:T(8,128)S(1)}, f32[64,128]{1,0:T(8,128)S(1)}, u32[]{:S(2)}, u32[]{:S(2)}) %collective-permute-start.27) | collective-permute-done | bytes 32800 | tf_op jit(solution)/shard_map/ppermute | solution.py:149
  83.1 3.4 %second.1 = (f32[64,64]{1,0:T(8,128)S(1)}, f32[64,64]{1,0:T(8,128)S(1)}, f32[128,192]{1,0:T(8,128)S(1)}, f32[64,64]{1,0:T(8,128)S(1)}) custom-call(f32[64,128]{1,0:T(8,128)S(1)} %add.58.gram_ref, f32[64,64]{1,0:T(8,128)S(1)} %first.1.inverse_ref), custom_call_target="tpu_custom_call" | custom-call | tf_op jit(solution)/shard_map/second/pallas_call | solution.py:604
  86.4 1.7 %blend.3 = (f32[16,64,128]{2,1,0:T(8,128)S(1)}, f32[16,64,128]{2,1,0:T(8,128)S(1)}, f32[64,64]{1,0:T(8,128)S(1)}) custom-call(s32[4]{0:T(128)S(1)} %pad_add_fusion.place_ref, f32[32,64,128]{2,1,0:T(8,128)S(1)} %get-tuple-element.123.refs_3_.x_ref, f32[32,32,128]{2,1,0:T(8,128)S(1)} %get-tuple-element.105.x_ref.a_ref, ...), custom_call_target="tpu_custom_call" | custom-call | tf_op jit(solution)/shard_map/blend/pallas_call | solution.py:448
  88.2 1.7 %blend.2 = (f32[16,64,128]{2,1,0:T(8,128)S(1)}, f32[16,64,128]{2,1,0:T(8,128)S(1)}, f32[64,64]{1,0:T(8,128)S(1)}) custom-call(s32[4]{0:T(128)S(1)} %pad_add_fusion.place_ref, f32[32,64,128]{2,1,0:T(8,128)S(1)} %get-tuple-element.123.refs_3_.x_ref, f32[32,32,128]{2,1,0:T(8,128)S(1)} %get-tuple-element.105.x_ref.a_ref, ...), custom_call_target="tpu_custom_call" | custom-call | tf_op jit(solution)/shard_map/blend/pallas_call | solution.py:448
  92.9 2.0 %third.1 = (f32[32,64,128]{2,1,0:T(8,128)S(1)}, f32[72,128]{1,0:T(8,128)S(1)}) custom-call(s32[4]{0:T(128)S(1)} %pad_add_fusion.place_ref, f32[16,32,128]{2,1,0:T(8,128)S(1)} %add.60.mine_ref, f32[16,32,128]{2,1,0:T(8,128)S(1)} %collective-permute-done.30.other_ref, f32[64,64]{1,0:T(8,128)S(1)} %get-tuple-element.138.gain_ref, ...), custom_call_target="tpu_custom_call" | custom-call | tf_op jit(solution)/shard_map/third/pallas_call | solution.py:611
  94.9 2.3 %collective-permute-start.33 = (f32[72,128]{1,0:T(8,128)S(1)}, f32[72,128]{1,0:T(8,128)S(1)}, u32[]{:S(2)}, u32[]{:S(2)}) collective-permute-start(f32[72,128]{1,0:T(8,128)S(1)} %get-tuple-element.144), channel_id=1, source_target_pairs={{0,12},{4,8},{8,4},{12,0},{1,13},{5,9},{9,5},{13,1},{2,14},{6,10},... | collective-permute-start | bytes 110600 | tf_op jit(solution)/shard_map/ppermute | solution.py:161
  97.2 1.9 %collective-permute-start.32 = (f32[72,128]{1,0:T(8,128)S(1)}, f32[72,128]{1,0:T(8,128)S(1)}, u32[]{:S(2)}, u32[]{:S(2)}) collective-permute-start(f32[72,128]{1,0:T(8,128)S(1)} %get-tuple-element.144), channel_id=1, source_target_pairs={{0,8},{4,12},{8,0},{12,4},{1,9},{5,13},{9,1},{13,5},{2,10},{6,14},... | collective-permute-start | bytes 110600 | tf_op jit(solution)/shard_map/ppermute | solution.py:161
  100.7 1.6 %collective-permute-done.32 = f32[72,128]{1,0:T(8,128)S(1)} collective-permute-done((f32[72,128]{1,0:T(8,128)S(1)}, f32[72,128]{1,0:T(8,128)S(1)}, u32[]{:S(2)}, u32[]{:S(2)}) %collective-permute-start.32) | collective-permute-done | bytes 36896 | tf_op jit(solution)/shard_map/ppermute | solution.py:161
  103.1 3.1 %fourth.1 = (f32[64,64]{1,0:T(8,128)S(1)}, f32[64,64]{1,0:T(8,128)S(1)}, f32[64,128]{1,0:T(8,128)S(1)}) custom-call(f32[72,128]{1,0:T(8,128)S(1)} %add_add_fusion.gram_ref), custom_call_target="tpu_custom_call" | custom-call | tf_op jit(solution)/shard_map/fourth/pallas_call | solution.py:619
  106.2 1.9 %last.1 = (f32[32,64,128]{2,1,0:T(8,128)}, f32[4,64,64]{2,1,0:T(8,128)}) custom-call(f32[32,64,128]{2,1,0:T(8,128)S(1)} %get-tuple-element.143.w_ref, f32[16,64,128]{2,1,0:T(8,128)S(1)} %get-tuple-element.141.refs_2_.low_ref, f32[16,64,128]{2,1,0:T(8,128)S(1)} %get-tuple-element.142.refs_3_.high_ref, f32[64,128]{1,0:T(8,128)S(1)} %get-tuple-element.145.coef_ref, ...), custom_call_target="tpu_custom_call" | custom-call | tf_op jit(solution)/shard_map/last/pallas_call | solution.py:622
  (87 shorter events, 34.4 us)
Async XLA Ops:
  0.6 8.8 %collective-permute-start.2 = (s32[1,1,44]{2,1,0:T(1,128)}, s32[1,1,44]{2,1,0:T(1,128)S(1)}, u32[]{:S(2)}, u32[]{:S(2)}) collective-permute-start(s32[1,1,44]{2,1,0:T(1,128)} %cols_ref.5), channel_id=1, source_target_pairs={{4,8},{0,12},{8,4},{12,0},{5,9},{1,13},{9,5},{13,1},{6,10},{2,14},... | collective-permute-start | bytes 536 | tf_op jit(solution)/shard_map/ppermute | solution.py:119
  5.8 3.7 %collective-permute-start.1 = (s32[1,1,44]{2,1,0:T(1,128)}, s32[1,1,44]{2,1,0:T(1,128)S(1)}, u32[]{:S(2)}, u32[]{:S(2)}) collective-permute-start(s32[1,1,44]{2,1,0:T(1,128)} %cols_ref.5), channel_id=1, source_target_pairs={{0,4},{8,12},{4,0},{12,8},{1,5},{9,13},{5,1},{13,9},{2,6},{10,14},... | collective-permute-start | bytes 536 | tf_op jit(solution)/shard_map/ppermute | solution.py:119
  5.8 4.6 %collective-permute-start = (s32[1,1,44]{2,1,0:T(1,128)}, s32[1,1,44]{2,1,0:T(1,128)S(1)}, u32[]{:S(2)}, u32[]{:S(2)}) collective-permute-start(s32[1,1,44]{2,1,0:T(1,128)} %cols_ref.5), channel_id=1, source_target_pairs={{0,8},{4,12},{8,0},{12,4},{1,9},{5,13},{9,1},{13,5},{2,10},{6,14},... | collective-permute-start | bytes 536 | tf_op jit(solution)/shard_map/ppermute | solution.py:119
  11.8 6.5 %collective-permute-start.5 = (f32[8,32,128]{2,1,0:T(8,128)S(1)}, f32[8,32,128]{2,1,0:T(8,128)S(1)}, u32[]{:S(2)}, u32[]{:S(2)}) collective-permute-start(f32[8,32,128]{2,1,0:T(8,128)S(1)} %get-tuple-element.81), channel_id=1, source_target_pairs={{0,4},{8,12},{4,0},{12,8},{1,5},{9,13},{5,1},{13,9},{2,6},{10,14},... | collective-permute-start | bytes 393224 | tf_op jit(solution)/shard_map/ppermute | solution.py:119
  13.6 14.3 %collective-permute-start.3 = (f32[8,32,128]{2,1,0:T(8,128)S(1)}, f32[8,32,128]{2,1,0:T(8,128)S(1)}, u32[]{:S(2)}, u32[]{:S(2)}) collective-permute-start(f32[8,32,128]{2,1,0:T(8,128)S(1)} %get-tuple-element.79), channel_id=1, source_target_pairs={{0,8},{4,12},{8,0},{12,4},{1,9},{5,13},{9,1},{13,5},{2,10},{6,14},... | collective-permute-start | bytes 393224 | tf_op jit(solution)/shard_map/ppermute | solution.py:119
  14.6 8.3 %collective-permute-start.4 = (f32[8,32,128]{2,1,0:T(8,128)S(1)}, f32[8,32,128]{2,1,0:T(8,128)S(1)}, u32[]{:S(2)}, u32[]{:S(2)}) collective-permute-start(f32[8,32,128]{2,1,0:T(8,128)S(1)} %get-tuple-element.80), channel_id=1, source_target_pairs={{4,8},{0,12},{8,4},{12,0},{5,9},{1,13},{9,5},{13,1},{6,10},{2,14},... | collective-permute-start | bytes 393224 | tf_op jit(solution)/shard_map/ppermute | solution.py:119
  19.8 8.0 %collective-permute-start.6 = (f32[64,64]{1,0:T(8,128)S(1)}, f32[64,64]{1,0:T(8,128)S(1)}, u32[]{:S(2)}, u32[]{:S(2)}) collective-permute-start(f32[64,64]{1,0:T(8,128)S(1)} %gram.1), channel_id=1, source_target_pairs={{0,4},{4,0},{8,12},{12,8},{1,5},{5,1},{9,13},{13,9},{2,6},{6,2},{1... | collective-permute-start | bytes 49160 | tf_op jit(solution)/shard_map/ppermute | solution.py:140
  23.9 9.5 %collective-permute-start.9 = (f32[8,32,128]{2,1,0:T(8,128)S(1)}, f32[8,32,128]{2,1,0:T(8,128)S(1)}, u32[]{:S(2)}, u32[]{:S(2)}) collective-permute-start(f32[8,32,128]{2,1,0:T(8,128)S(1)} %get-tuple-element.95), channel_id=1, source_target_pairs={{0,4},{8,12},{4,0},{12,8},{1,5},{9,13},{5,1},{13,9},{2,6},{10,14},... | collective-permute-start | bytes 393224 | tf_op jit(solution)/shard_map/ppermute | solution.py:119
  27.8 11.2 %collective-permute-start.10 = (f32[64,64]{1,0:T(8,128)S(1)}, f32[64,64]{1,0:T(8,128)S(1)}, u32[]{:S(2)}, u32[]{:S(2)}) collective-permute-start(f32[64,64]{1,0:T(8,128)S(1)} %add.49), channel_id=1, source_target_pairs={{0,8},{4,12},{8,0},{12,4},{1,9},{5,13},{9,1},{13,5},{2,10},{6,14},... | collective-permute-start | bytes 49160 | tf_op jit(solution)/shard_map/ppermute | solution.py:149
  29.0 14.5 %collective-permute-start.7 = (f32[8,32,128]{2,1,0:T(8,128)S(1)}, f32[8,32,128]{2,1,0:T(8,128)S(1)}, u32[]{:S(2)}, u32[]{:S(2)}) collective-permute-start(f32[8,32,128]{2,1,0:T(8,128)S(1)} %get-tuple-element.92), channel_id=1, source_target_pairs={{0,8},{4,12},{8,0},{12,4},{1,9},{5,13},{9,1},{13,5},{2,10},{6,14},... | collective-permute-start | bytes 393224 | tf_op jit(solution)/shard_map/ppermute | solution.py:119
  31.6 9.9 %collective-permute-start.8 = (f32[8,32,128]{2,1,0:T(8,128)S(1)}, f32[8,32,128]{2,1,0:T(8,128)S(1)}, u32[]{:S(2)}, u32[]{:S(2)}) collective-permute-start(f32[8,32,128]{2,1,0:T(8,128)S(1)} %get-tuple-element.94), channel_id=1, source_target_pairs={{4,8},{0,12},{8,4},{12,0},{5,9},{1,13},{9,5},{13,1},{6,10},{2,14},... | collective-permute-start | bytes 393224 | tf_op jit(solution)/shard_map/ppermute | solution.py:119
  35.0 8.4 %collective-permute-start.13 = (f32[16,32,128]{2,1,0:T(8,128)S(1)}, f32[16,32,128]{2,1,0:T(8,128)S(1)}, u32[]{:S(2)}, u32[]{:S(2)}) collective-permute-start(f32[16,32,128]{2,1,0:T(8,128)S(1)} %add.50), channel_id=1, source_target_pairs={{0,2},{1,3},{2,0},{3,1},{4,6},{5,7},{6,4},{7,5},{8,10},{9,11},{10,... | collective-permute-start | bytes 786440 | tf_op jit(solution)/shard_map/ppermute | solution.py:514
  43.4 1.7 %collective-permute-start.14 = (f32[16,32,128]{2,1,0:T(8,128)S(1)}, f32[16,32,128]{2,1,0:T(8,128)S(1)}, u32[]{:S(2)}, u32[]{:S(2)}) collective-permute-start(f32[16,32,128]{2,1,0:T(8,128)S(1)} %add.52.refs_3_), channel_id=1, source_target_pairs={{0,1},{1,0},{2,3},{3,2},{4,5},{5,4},{6,7},{7,6},{8,9},{9,8},{10,11... | collective-permute-start | bytes 786440 | tf_op jit(solution)/shard_map/ppermute | solution.py:576
  44.6 2.0 %collective-permute-start.12 = (f32[16,32,128]{2,1,0:T(8,128)S(1)}, f32[16,32,128]{2,1,0:T(8,128)S(1)}, u32[]{:S(2)}, u32[]{:S(2)}) collective-permute-start(f32[16,32,128]{2,1,0:T(8,128)S(1)} %get-tuple-element.102), channel_id=1, source_target_pairs={{0,1},{1,0},{2,3},{3,2},{4,5},{5,4},{6,7},{7,6},{8,9},{9,8},{10,11... | collective-permute-start | bytes 786440 | tf_op jit(solution)/shard_map/ppermute | solution.py:580
  46.6 8.3 %collective-permute-start.15 = (f32[16,32,128]{2,1,0:T(8,128)S(1)}, f32[16,32,128]{2,1,0:T(8,128)S(1)}, u32[]{:S(2)}, u32[]{:S(2)}) collective-permute-start(f32[16,32,128]{2,1,0:T(8,128)S(1)} %add.53), channel_id=1, source_target_pairs={{0,2},{1,3},{2,0},{3,1},{4,6},{5,7},{6,4},{7,5},{8,10},{9,11},{10,... | collective-permute-start | bytes 786440 | tf_op jit(solution)/shard_map/ppermute | solution.py:514
  48.2 10.7 %collective-permute-start.17 = (f32[8,32,128]{2,1,0:T(8,128)S(1)}, f32[8,32,128]{2,1,0:T(8,128)S(1)}, u32[]{:S(2)}, u32[]{:S(2)}) collective-permute-start(f32[8,32,128]{2,1,0:T(8,128)S(1)} %get-tuple-element.110), channel_id=1, source_target_pairs={{0,8},{4,12},{8,0},{12,4},{1,9},{5,13},{9,1},{13,5},{2,10},{6,14},... | collective-permute-start | bytes 393224 | tf_op jit(solution)/shard_map/ppermute | solution.py:119
  50.4 12.0 %collective-permute-start.21 = (f32[8,32,128]{2,1,0:T(8,128)S(1)}, f32[8,32,128]{2,1,0:T(8,128)S(1)}, u32[]{:S(2)}, u32[]{:S(2)}) collective-permute-start(f32[8,32,128]{2,1,0:T(8,128)S(1)} %get-tuple-element.117), channel_id=1, source_target_pairs={{0,4},{8,12},{4,0},{12,8},{1,5},{9,13},{5,1},{13,9},{2,6},{10,14},... | collective-permute-start | bytes 393224 | tf_op jit(solution)/shard_map/ppermute | solution.py:119
  51.9 9.5 %collective-permute-start.22 = (f32[8,32,128]{2,1,0:T(8,128)S(1)}, f32[8,32,128]{2,1,0:T(8,128)S(1)}, u32[]{:S(2)}, u32[]{:S(2)}) collective-permute-start(f32[8,32,128]{2,1,0:T(8,128)S(1)} %get-tuple-element.118), channel_id=1, source_target_pairs={{4,8},{0,12},{8,4},{12,0},{5,9},{1,13},{9,5},{13,1},{6,10},{2,14},... | collective-permute-start | bytes 393224 | tf_op jit(solution)/shard_map/ppermute | solution.py:119
  55.0 4.8 %collective-permute-start.16 = (f32[16,32,128]{2,1,0:T(8,128)S(1)}, f32[16,32,128]{2,1,0:T(8,128)S(1)}, u32[]{:S(2)}, u32[]{:S(2)}) collective-permute-start(f32[16,32,128]{2,1,0:T(8,128)S(1)} %add.54.refs_3_), channel_id=1, source_target_pairs={{0,1},{1,0},{2,3},{3,2},{4,5},{5,4},{6,7},{7,6},{8,9},{9,8},{10,11... | collective-permute-start | bytes 786440 | tf_op jit(solution)/shard_map/ppermute | solution.py:584
  61.3 8.1 %collective-permute-start.20 = (f32[8,32,128]{2,1,0:T(8,128)S(1)}, f32[8,32,128]{2,1,0:T(8,128)S(1)}, u32[]{:S(2)}, u32[]{:S(2)}) collective-permute-start(f32[8,32,128]{2,1,0:T(8,128)S(1)} %get-tuple-element.115), channel_id=1, source_target_pairs={{0,4},{8,12},{4,0},{12,8},{1,5},{9,13},{5,1},{13,9},{2,6},{10,14},... | collective-permute-start | bytes 393224 | tf_op jit(solution)/shard_map/ppermute | solution.py:119
  63.5 12.4 %collective-permute-start.18 = (f32[8,32,128]{2,1,0:T(8,128)S(1)}, f32[8,32,128]{2,1,0:T(8,128)S(1)}, u32[]{:S(2)}, u32[]{:S(2)}) collective-permute-start(f32[8,32,128]{2,1,0:T(8,128)S(1)} %get-tuple-element.113), channel_id=1, source_target_pairs={{0,8},{4,12},{8,0},{12,4},{1,9},{5,13},{9,1},{13,5},{2,10},{6,14},... | collective-permute-start | bytes 393224 | tf_op jit(solution)/shard_map/ppermute | solution.py:119
  65.3 8.1 %collective-permute-start.19 = (f32[8,32,128]{2,1,0:T(8,128)S(1)}, f32[8,32,128]{2,1,0:T(8,128)S(1)}, u32[]{:S(2)}, u32[]{:S(2)}) collective-permute-start(f32[8,32,128]{2,1,0:T(8,128)S(1)} %get-tuple-element.114), channel_id=1, source_target_pairs={{4,8},{0,12},{8,4},{12,0},{5,9},{1,13},{9,5},{13,1},{6,10},{2,14},... | collective-permute-start | bytes 393224 | tf_op jit(solution)/shard_map/ppermute | solution.py:119
  67.6 2.7 %collective-permute-start.23 = (f32[16,32,128]{2,1,0:T(8,128)S(1)}, f32[16,32,128]{2,1,0:T(8,128)S(1)}, u32[]{:S(2)}, u32[]{:S(2)}) collective-permute-start(f32[16,32,128]{2,1,0:T(8,128)S(1)} %get-tuple-element.124), channel_id=1, source_target_pairs={{0,1},{1,0},{2,3},{3,2},{4,5},{5,4},{6,7},{7,6},{8,9},{9,8},{10,11... | collective-permute-start | bytes 786440 | tf_op jit(solution)/shard_map/ppermute | solution.py:590
  71.4 4.5 %collective-permute-start.24 = (f32[64,128]{1,0:T(8,128)S(1)}, f32[64,128]{1,0:T(8,128)S(1)}, u32[]{:S(2)}, u32[]{:S(2)}) collective-permute-start(f32[64,128]{1,0:T(8,128)S(1)} %cross.1), channel_id=1, source_target_pairs={{0,4},{4,0},{8,12},{12,8},{1,5},{5,1},{9,13},{13,9},{2,6},{6,2},{1... | collective-permute-start | bytes 98312 | tf_op jit(solution)/shard_map/ppermute | solution.py:140
  71.5 10.8 %collective-permute-start.26 = (f32[16,32,128]{2,1,0:T(8,128)S(1)}, f32[16,32,128]{2,1,0:T(8,128)S(1)}, u32[]{:S(2)}, u32[]{:S(2)}) collective-permute-start(f32[16,32,128]{2,1,0:T(8,128)S(1)} %add.55), channel_id=1, source_target_pairs={{0,2},{1,3},{2,0},{3,1},{4,6},{5,7},{6,4},{7,5},{8,10},{9,11},{10,... | collective-permute-start | bytes 786440 | tf_op jit(solution)/shard_map/ppermute | solution.py:514
  77.0 5.4 %collective-permute-start.25 = (f32[16,32,128]{2,1,0:T(8,128)S(1)}, f32[16,32,128]{2,1,0:T(8,128)S(1)}, u32[]{:S(2)}, u32[]{:S(2)}) collective-permute-start(f32[16,32,128]{2,1,0:T(8,128)S(1)} %get-tuple-element.130), channel_id=1, source_target_pairs={{0,1},{1,0},{2,3},{3,2},{4,5},{5,4},{6,7},{7,6},{8,9},{9,8},{10,11... | collective-permute-start | bytes 786440 | tf_op jit(solution)/shard_map/ppermute | solution.py:599
  77.1 5.2 %collective-permute-start.27 = (f32[64,128]{1,0:T(8,128)S(1)}, f32[64,128]{1,0:T(8,128)S(1)}, u32[]{:S(2)}, u32[]{:S(2)}) collective-permute-start(f32[64,128]{1,0:T(8,128)S(1)} %add.56), channel_id=1, source_target_pairs={{0,8},{4,12},{8,0},{12,4},{1,9},{5,13},{9,1},{13,5},{2,10},{6,14},... | collective-permute-start | bytes 98312 | tf_op jit(solution)/shard_map/ppermute | solution.py:149
  82.3 4.1 %collective-permute-start.29 = (f32[16,32,128]{2,1,0:T(8,128)S(1)}, f32[16,32,128]{2,1,0:T(8,128)S(1)}, u32[]{:S(2)}, u32[]{:S(2)}) collective-permute-start(f32[16,32,128]{2,1,0:T(8,128)S(1)} %add.57.mine_ref), channel_id=1, source_target_pairs={{0,1},{1,0},{2,3},{3,2},{4,5},{5,4},{6,7},{7,6},{8,9},{9,8},{10,11... | collective-permute-start | bytes 786440 | tf_op jit(solution)/shard_map/ppermute | solution.py:601
  82.5 8.8 %collective-permute-start.28 = (f32[16,32,128]{2,1,0:T(8,128)S(1)}, f32[16,32,128]{2,1,0:T(8,128)S(1)}, u32[]{:S(2)}, u32[]{:S(2)}) collective-permute-start(f32[16,32,128]{2,1,0:T(8,128)S(1)} %add.59), channel_id=1, source_target_pairs={{0,2},{1,3},{2,0},{3,1},{4,6},{5,7},{6,4},{7,5},{8,10},{9,11},{10,... | collective-permute-start | bytes 786440 | tf_op jit(solution)/shard_map/ppermute | solution.py:514
  94.9 5.8 %collective-permute-start.33 = (f32[72,128]{1,0:T(8,128)S(1)}, f32[72,128]{1,0:T(8,128)S(1)}, u32[]{:S(2)}, u32[]{:S(2)}) collective-permute-start(f32[72,128]{1,0:T(8,128)S(1)} %get-tuple-element.144), channel_id=1, source_target_pairs={{0,12},{4,8},{8,4},{12,0},{1,13},{5,9},{9,5},{13,1},{2,14},{6,10},... | collective-permute-start | bytes 110600 | tf_op jit(solution)/shard_map/ppermute | solution.py:161
  97.2 5.1 %collective-permute-start.32 = (f32[72,128]{1,0:T(8,128)S(1)}, f32[72,128]{1,0:T(8,128)S(1)}, u32[]{:S(2)}, u32[]{:S(2)}) collective-permute-start(f32[72,128]{1,0:T(8,128)S(1)} %get-tuple-element.144), channel_id=1, source_target_pairs={{0,8},{4,12},{8,0},{12,4},{1,9},{5,13},{9,1},{13,5},{2,10},{6,14},... | collective-permute-start | bytes 110600 | tf_op jit(solution)/shard_map/ppermute | solution.py:161
  99.1 4.0 %collective-permute-start.31 = (f32[72,128]{1,0:T(8,128)S(1)}, f32[72,128]{1,0:T(8,128)S(1)}, u32[]{:S(2)}, u32[]{:S(2)}) collective-permute-start(f32[72,128]{1,0:T(8,128)S(1)} %get-tuple-element.144), channel_id=1, source_target_pairs={{0,4},{4,0},{8,12},{12,8},{1,5},{5,1},{9,13},{13,9},{2,6},{6,2},{1... | collective-permute-start | bytes 110600 | tf_op jit(solution)/shard_map/ppermute | solution.py:161
  (6 other events, 31.0 us)

commit v16 on v15

--- a/solution.py
+++ b/solution.py
@@ -330,7 +330,7 @@
             [(outs[p],) for p in range(count)],
         )
         first = (place_ref[0] == 0).astype(F32)
-        acc_ref[...] = y_ref[...] * ((diag_ref[...] - SHIFT) * first)[:, None, :]
+        acc_ref[...] = y_ref[...] * (diag_ref[...] * first)[:, None, :]
 
     def join_rounds(members, place_ref, rows_ref, counts_ref, asked_refs, got_refs, split_ref, acc_ref):
         for n, p in enumerate(members):
@@ -410,13 +410,13 @@
     def lower_part():
         return lax.broadcasted_iota(jnp.int32, square, 0) >= lax.broadcasted_iota(jnp.int32, square, 1)
 
-    def second_body(gram_ref, inverse_ref, cross_ref, lower_ref, coef_ref, gain_ref):
+    def second_body(gram_ref, inverse_ref, shift_ref, cross_ref, lower_ref, coef_ref, gain_ref):
         start_inv = inverse_ref[...]
         cross = dot(dot(start_inv, gram_ref[:, :width]), start_inv, tb=True)
         applied = dot(dot(start_inv, gram_ref[:, width:]), start_inv, tb=True)
         upper, inverse = factor(applied - dot(cross, cross, tb=True))
         lower = upper.T
-        cross_ref[...] = cross + SHIFT * identity()
+        cross_ref[...] = cross + shift_ref[:1, :width] * identity()
         lower_ref[...] = lower
         gain = dot(inverse, start_inv)
         back = -dot(dot(inverse, cross), start_inv)
@@ -474,18 +474,18 @@
             jnp.sum(norm * identity(), axis=0, keepdims=True), (8, width)
         )
 
-    def fourth_body(gram_ref, cross_ref, lower_ref, coef_ref):
+    def fourth_body(gram_ref, shift_ref, cross_ref, lower_ref, coef_ref):
         cross = gram_ref[:width, :width]
         packed = gram_ref[:width, width:]
         flipped = packed.T
         squares = jnp.where(lower_part(), packed, flipped)
         norm = jnp.where(lower_part(), flipped, packed)
         norm = jnp.where(identity() > 0, gram_ref[width : width + 1, :width], norm)
-        taken = cross + SHIFT * (norm - identity())
+        taken = cross + shift_ref[:1, :width] * (norm - identity())
         mixed = dot(taken, cross, tb=True)
         squared = squares - mixed - mixed.T + dot(dot(taken, norm), taken, tb=True)
         upper, inverse = factor(squared)
-        cross_ref[...] = taken + SHIFT * identity()
+        cross_ref[...] = taken + shift_ref[:1, :width] * identity()
         lower_ref[...] = upper.T
         scale = math.sqrt(rows * length * peers)
         coef_ref[:, :width] = inverse * scale
@@ -522,7 +522,7 @@
             [chunk, chunk] + [packet] * count,
             [SMEM] * (3 + count) + [VMEM] * 4,
             name="resend",
-        )(place, tile_rows, slot_counts, *asked, mine, other, diagonal, split)
+        )(place, tile_rows, slot_counts, *asked, mine, other, centered, split)
         return y, acc, spread(sent)
 
     def own(y, *accs):
@@ -551,6 +551,10 @@
     )(place, tile_rows, slot_counts, *asked, x, split)
     got_a = spread(sent[:count])
     sent_b = list(sent[count:])
+    shift = end_sum(start_sum(jnp.full((8, length), jnp.mean(diagonal), F32), "res"), "res") / peers
+    centered = diagonal - shift[:1]
+    scaled = jnp.where(place[0] == 0, centered, 0.0)[:, None, :]
+    acc_a, acc_b = x[:, :part] * scaled, x[:, part:] * scaled
     acc_a, acc_b = own(x, after(acc_a, sent[0]), acc_b)
     for n in range(2):
         acc_a = join(acc_a, got_a, groups[n])
@@ -602,8 +606,8 @@
     cross_gram = end_sum(cross_gram, "res")
     mine_b = keep_b + after(core, mine_a, cross_gram)
     cross1, lower1, coef, gain = call(
-        second_body, [square, square, (2 * width, 3 * width), square], [VMEM] * 2, name="second"
-    )(after(cross_gram, mine_b), start_inv)
+        second_body, [square, square, (2 * width, 3 * width), square], [VMEM] * 3, name="second"
+    )(after(cross_gram, mine_b), start_inv, shift)
     w_low, q_low, norm_low = blend(0, mine_a, other_a, coef)
     w_high, q_high, norm_high = blend(1, mine_a, other_a, coef)
     mine_b = across(mine_b, norm_low, norm_high)
@@ -617,8 +621,8 @@
     )(place, mine_b, other_b, gain, w_low, w_high, q_low, q_high, norm_low, norm_high)
     gram = all_sum(gram, "res")
     cross2, lower2, coef = call(
-        fourth_body, [square, square, (width, 2 * width)], [VMEM], name="fourth"
-    )(gram)
+        fourth_body, [square, square, (width, 2 * width)], [VMEM] * 2, name="fourth"
+    )(gram, shift)
     return call(last_body, [full, (4, width, width)], [VMEM] * 8, name="last")(
         w, q_low, q_high, coef, cross1, lower1, cross2, lower2
     )

time: 108 us -> 116 us (1.074)
  waiting for transfers between devices: 22.4 us -> 26.5 us
  other arithmetic: 0.43 us -> 1.88 us
    ppermute x4, waiting for transfers between devices: 2.92 us -> 5.43 us  [across(): got = lax.ppermute(mine, 'vec', [(i, i ^ step) for i in range(lanes)])]
    ppermute x2 -> x3, waiting for transfers between devices: 4.45 us -> 1.99 us  [end_sum(): got = lax.ppermute(block, axis, [(i, i ^ step) for i in range(size)])]
    ppermute x15, starting transfers between devices: 27.2 us -> 25 us  [exchange(): lax.ppermute(block, axis, [(a, b) for a, b in pairs] + [(b, a) for a, b i...]
    ppermute x2 -> x3, starting transfers between devices: 3.36 us -> 5.47 us  [end_sum(): got = lax.ppermute(block, axis, [(i, i ^ step) for i in range(size)])]
    ppermute x15, waiting for transfers between devices: 7.57 us -> 9.66 us  [exchange(): lax.ppermute(block, axis, [(a, b) for a, b in pairs] + [(b, a) for a, b i...]
    ppermute x2 -> x3, waiting for transfers between devices: 1.59 us -> 3.5 us  [start_sum(): lax.ppermute(block, axis, [(i, i ^ step) for i in range(size)])]
    reduce_sum x0 -> x1, other arithmetic: none -> 1.32 us  [local(): jnp.mean(diagonal)]
  transfers between devices with their start and end apart: 34 -> 36, of which waited for: 15 -> 18; matrix products, arithmetic and copies ran while one was open for 1% -> 2% of each run, Pallas kernels for 31% -> 30%
where the time goes in v16:
time: 116 us; the launch traced here: 115 us
  Pallas kernels  42.7 us (37%)
  starting transfers between devices  41.6 us (36%)
  waiting for transfers between devices  26.5 us (23%)
  other arithmetic  1.88 us (2%)
  between operations  1.78 us (2%)
    ppermute x15, starting transfers between devices, exchange(): lax.ppermute(block, axis, [(a, b) for a, b in pairs] + [(b, a) for a, b i...  25 us
    pallas_call x12, Pallas kernels, join(): call(body, [halfchunk] * 2 if last else [chunk], [SMEM] * (3 + size) + [V...  11.9 us
    ppermute x15, waiting for transfers between devices, exchange(): lax.ppermute(block, axis, [(a, b) for a, b in pairs] + [(b, a) for a, b i...  9.66 us
    ppermute x3, starting transfers between devices, end_sum(): got = lax.ppermute(block, axis, [(i, i ^ step) for i in range(size)])  5.47 us
    pallas_call x3, Pallas kernels, own(): call(own_body, [chunk] * len(accs), [SMEM] * 2 + [VMEM] * (2 + len(accs))...  5.46 us
    ppermute x4, waiting for transfers between devices, across(): got = lax.ppermute(mine, 'vec', [(i, i ^ step) for i in range(lanes)])  5.43 us
    ppermute x3, starting transfers between devices, all_sum(): lax.ppermute(block, axis, [(i, i ^ m) for i in range(size)])  4.42 us
    ppermute x4, starting transfers between devices, across(): got = lax.ppermute(mine, 'vec', [(i, i ^ step) for i in range(lanes)])  4.23 us
  transfers between devices with their start and end apart: 36, of which 18 were waited for; matrix products, arithmetic and copies ran while one was open for 2% of the time, Pallas kernels for 30%

profile of v16, /device:TPU:0, one launch (start us, length us, event | category | flops | bytes accessed | tf_op | source)
XLA Modules:
  0.0 115.3 jit_solution(17549902180212532490)
XLA Ops:
  0.6 5.1 %collective-permute-start.2 = (s32[1,1,44]{2,1,0:T(1,128)}, s32[1,1,44]{2,1,0:T(1,128)S(1)}, u32[]{:S(2)}, u32[]{:S(2)}) collective-permute-start(s32[1,1,44]{2,1,0:T(1,128)} %cols_ref.5), channel_id=1, source_target_pairs={{4,8},{0,12},{8,4},{12,0},{5,9},{1,13},{9,5},{13,1},{6,10},{2,14},... | collective-permute-start | bytes 536 | tf_op jit(solution)/shard_map/ppermute | solution.py:119
  10.5 1.5 %collective-permute-done.6 = f32[8,128]{1,0:T(8,128)S(1)} collective-permute-done((f32[8,128]{1,0:T(8,128)S(1)}, f32[8,128]{1,0:T(8,128)S(1)}, u32[]{:S(2)}, u32[]{:S(2)}) %collective-permute-start.6) | collective-permute-done | bytes 4128 | tf_op jit(solution)/shard_map/ppermute | solution.py:140
  12.1 2.3 %collective-permute-start.7 = (f32[8,128]{1,0:T(8,128)S(1)}, f32[8,128]{1,0:T(8,128)S(1)}, u32[]{:S(2)}, u32[]{:S(2)}) collective-permute-start(f32[8,128]{1,0:T(8,128)S(1)} %broadcast_add_fusion), channel_id=1, source_target_pairs={{0,8},{4,12},{8,0},{12,4},{1,9},{5,13},{9,1},{13,5},{2,10},{6,14},... | collective-permute-start | bytes 12296 | tf_op jit(solution)/shard_map/ppermute | solution.py:149
  14.4 3.2 %prepare.1 = (f32[32,64,128]{2,1,0:T(8,128)S(1)}, bf16[44,2,128,128]{3,2,1,0:T(8,128)(2,1)S(1)}, f32[32,32,128]{2,1,0:T(8,128)}, f32[32,32,128]{2,1,0:T(8,128)}) custom-call(f32[32,64,128]{2,1,0:T(8,128)} %x_hbm.1, f32[32,128]{1,0:T(8,128)} %diag_hbm.1, f32[1,1,44,128,128]{4,3,2,1,0:T(8,128)} %tiles_hbm.1), custom_call_target="tpu_custom_call" | custom-call | tf_op jit(solution)/shard_map/prepare/pallas_call | solution.py:538
  19.4 4.0 %collective-permute-start.4 = (f32[8,32,128]{2,1,0:T(8,128)S(1)}, f32[8,32,128]{2,1,0:T(8,128)S(1)}, u32[]{:S(2)}, u32[]{:S(2)}) collective-permute-start(f32[8,32,128]{2,1,0:T(8,128)S(1)} %get-tuple-element.78), channel_id=1, source_target_pairs={{4,8},{0,12},{8,4},{12,0},{5,9},{1,13},{9,5},{13,1},{6,10},{2,14},... | collective-permute-start | bytes 393224 | tf_op jit(solution)/shard_map/ppermute | solution.py:119
  23.6 2.0 %own.3 = (f32[32,32,128]{2,1,0:T(8,128)S(1)}, f32[32,32,128]{2,1,0:T(8,128)S(1)}) custom-call(s32[1,1,44]{2,1,0:T(1,128)S(1)} %copy-done, s32[1,1,44]{2,1,0:T(1,128)S(1)} %copy-done.1, f32[32,64,128]{2,1,0:T(8,128)S(1)} %get-tuple-element.119.refs_3_.x_ref, ...), custom_call_target="tpu_custom_call", output_to_operand_aliasing={{0}: (4, {}), {1}: (5, {})} | custom-call | tf_op jit(solution)/shard_map/own/pallas_call | solution.py:529
  25.6 4.9 %collective-permute-done.5.refs_1_ = f32[8,32,128]{2,1,0:T(8,128)S(1)} collective-permute-done((f32[8,32,128]{2,1,0:T(8,128)S(1)}, f32[8,32,128]{2,1,0:T(8,128)S(1)}, u32[]{:S(2)}, u32[]{:S(2)}) %collective-permute-start.5) | collective-permute-done | bytes 131104 | tf_op jit(solution)/shard_map/ppermute | solution.py:119
  33.0 2.1 %collective-permute-start.11 = (f32[8,32,128]{2,1,0:T(8,128)S(1)}, f32[8,32,128]{2,1,0:T(8,128)S(1)}, u32[]{:S(2)}, u32[]{:S(2)}) collective-permute-start(f32[8,32,128]{2,1,0:T(8,128)S(1)} %get-tuple-element.91), channel_id=1, source_target_pairs={{0,4},{8,12},{4,0},{12,8},{1,5},{9,13},{5,1},{13,9},{2,6},{10,14},... | collective-permute-start | bytes 393224 | tf_op jit(solution)/shard_map/ppermute | solution.py:119
  37.1 2.6 %collective-permute-start.9 = (f32[8,32,128]{2,1,0:T(8,128)S(1)}, f32[8,32,128]{2,1,0:T(8,128)S(1)}, u32[]{:S(2)}, u32[]{:S(2)}) collective-permute-start(f32[8,32,128]{2,1,0:T(8,128)S(1)} %get-tuple-element.88), channel_id=1, source_target_pairs={{0,8},{4,12},{8,0},{12,4},{1,9},{5,13},{9,1},{13,5},{2,10},{6,14},... | collective-permute-start | bytes 393224 | tf_op jit(solution)/shard_map/ppermute | solution.py:119
  42.6 1.5 %collective-permute-start.15 = (f32[16,32,128]{2,1,0:T(8,128)S(1)}, f32[16,32,128]{2,1,0:T(8,128)S(1)}, u32[]{:S(2)}, u32[]{:S(2)}) collective-permute-start(f32[16,32,128]{2,1,0:T(8,128)S(1)} %add.58), channel_id=1, source_target_pairs={{0,2},{1,3},{2,0},{3,1},{4,6},{5,7},{6,4},{7,5},{8,10},{9,11},{10,... | collective-permute-start | bytes 786440 | tf_op jit(solution)/shard_map/ppermute | solution.py:514
  44.2 2.4 %first.1.inverse_ref = f32[64,64]{1,0:T(8,128)S(1)} custom-call(f32[64,64]{1,0:T(8,128)S(1)} %add.59.gram_ref), custom_call_target="tpu_custom_call" | custom-call | tf_op jit(solution)/shard_map/first/pallas_call | solution.py:577
  47.6 3.5 %collective-permute-done.15 = f32[16,32,128]{2,1,0:T(8,128)S(1)} collective-permute-done((f32[16,32,128]{2,1,0:T(8,128)S(1)}, f32[16,32,128]{2,1,0:T(8,128)S(1)}, u32[]{:S(2)}, u32[]{:S(2)}) %collective-permute-start.15) | collective-permute-done | bytes 262176 | tf_op jit(solution)/shard_map/ppermute | solution.py:514
  55.8 1.7 %own.4.refs_3_ = f32[32,32,128]{2,1,0:T(8,128)S(1)} custom-call(s32[1,1,44]{2,1,0:T(1,128)S(1)} %copy-done, s32[1,1,44]{2,1,0:T(1,128)S(1)} %copy-done.1, f32[32,32,128]{2,1,0:T(8,128)S(1)} %get-tuple-element.101.x_ref.a_ref, bf16[44,2,128,128]{3,2,1,0:T(8,128)(2,1)S(1)} %get-tuple-element.75.refs_4_.split_ref.refs_2_.refs_6_, ...), custom_call_target="tpu_custom_call", output_to_operand_aliasing={{}: (4, {})} | custom-call | tf_op jit(solution)/shard_map/own/pallas_call | solution.py:529
  57.5 2.5 %collective-permute-start.23 = (f32[8,32,128]{2,1,0:T(8,128)S(1)}, f32[8,32,128]{2,1,0:T(8,128)S(1)}, u32[]{:S(2)}, u32[]{:S(2)}) collective-permute-start(f32[8,32,128]{2,1,0:T(8,128)S(1)} %get-tuple-element.113), channel_id=1, source_target_pairs={{0,4},{8,12},{4,0},{12,8},{1,5},{9,13},{5,1},{13,9},{2,6},{10,14},... | collective-permute-start | bytes 393224 | tf_op jit(solution)/shard_map/ppermute | solution.py:119
  60.0 2.0 %collective-permute-start.24 = (f32[8,32,128]{2,1,0:T(8,128)S(1)}, f32[8,32,128]{2,1,0:T(8,128)S(1)}, u32[]{:S(2)}, u32[]{:S(2)}) collective-permute-start(f32[8,32,128]{2,1,0:T(8,128)S(1)} %get-tuple-element.114), channel_id=1, source_target_pairs={{4,8},{0,12},{8,4},{12,0},{5,9},{1,13},{9,5},{13,1},{6,10},{2,14},... | collective-permute-start | bytes 393224 | tf_op jit(solution)/shard_map/ppermute | solution.py:119
  62.7 2.1 %collective-permute-done.19.refs_1_ = f32[8,32,128]{2,1,0:T(8,128)S(1)} collective-permute-done((f32[8,32,128]{2,1,0:T(8,128)S(1)}, f32[8,32,128]{2,1,0:T(8,128)S(1)}, u32[]{:S(2)}, u32[]{:S(2)}) %collective-permute-start.19) | collective-permute-done | bytes 131104 | tf_op jit(solution)/shard_map/ppermute | solution.py:119
  70.2 2.3 %collective-permute-start.20 = (f32[8,32,128]{2,1,0:T(8,128)S(1)}, f32[8,32,128]{2,1,0:T(8,128)S(1)}, u32[]{:S(2)}, u32[]{:S(2)}) collective-permute-start(f32[8,32,128]{2,1,0:T(8,128)S(1)} %get-tuple-element.109), channel_id=1, source_target_pairs={{0,8},{4,12},{8,0},{12,4},{1,9},{5,13},{9,1},{13,5},{2,10},{6,14},... | collective-permute-start | bytes 393224 | tf_op jit(solution)/shard_map/ppermute | solution.py:119
  72.5 2.2 %collective-permute-start.21 = (f32[8,32,128]{2,1,0:T(8,128)S(1)}, f32[8,32,128]{2,1,0:T(8,128)S(1)}, u32[]{:S(2)}, u32[]{:S(2)}) collective-permute-start(f32[8,32,128]{2,1,0:T(8,128)S(1)} %get-tuple-element.110), channel_id=1, source_target_pairs={{4,8},{0,12},{8,4},{12,0},{5,9},{1,13},{9,5},{13,1},{6,10},{2,14},... | collective-permute-start | bytes 393224 | tf_op jit(solution)/shard_map/ppermute | solution.py:119
  74.7 1.7 %own.5.refs_3_ = f32[32,32,128]{2,1,0:T(8,128)S(1)} custom-call(s32[1,1,44]{2,1,0:T(1,128)S(1)} %copy-done, s32[1,1,44]{2,1,0:T(1,128)S(1)} %copy-done.1, f32[32,32,128]{2,1,0:T(8,128)S(1)} %get-tuple-element.122.x_ref.b_ref, bf16[44,2,128,128]{3,2,1,0:T(8,128)(2,1)S(1)} %get-tuple-element.75.refs_4_.split_ref.refs_2_.refs_6_, ...), custom_call_target="tpu_custom_call", output_to_operand_aliasing={{}: (4, {})} | custom-call | tf_op jit(solution)/shard_map/own/pallas_call | solution.py:529
  79.2 1.8 %collective-permute-done.21.refs_1_ = f32[8,32,128]{2,1,0:T(8,128)S(1)} collective-permute-done((f32[8,32,128]{2,1,0:T(8,128)S(1)}, f32[8,32,128]{2,1,0:T(8,128)S(1)}, u32[]{:S(2)}, u32[]{:S(2)}) %collective-permute-start.21) | collective-permute-done | bytes 131104 | tf_op jit(solution)/shard_map/ppermute | solution.py:119
  84.3 3.1 %collective-permute-start.29 = (f32[64,128]{1,0:T(8,128)S(1)}, f32[64,128]{1,0:T(8,128)S(1)}, u32[]{:S(2)}, u32[]{:S(2)}) collective-permute-start(f32[64,128]{1,0:T(8,128)S(1)} %add.64), channel_id=1, source_target_pairs={{0,8},{4,12},{8,0},{12,4},{1,9},{5,13},{9,1},{13,5},{2,10},{6,14},... | collective-permute-start | bytes 98312 | tf_op jit(solution)/shard_map/ppermute | solution.py:149
  87.4 2.0 %collective-permute-done.29 = f32[64,128]{1,0:T(8,128)S(1)} collective-permute-done((f32[64,128]{1,0:T(8,128)S(1)}, f32[64,128]{1,0:T(8,128)S(1)}, u32[]{:S(2)}, u32[]{:S(2)}) %collective-permute-start.29) | collective-permute-done | bytes 32800 | tf_op jit(solution)/shard_map/ppermute | solution.py:149
  90.2 3.4 %second.1 = (f32[64,64]{1,0:T(8,128)S(1)}, f32[64,64]{1,0:T(8,128)S(1)}, f32[128,192]{1,0:T(8,128)S(1)}, f32[64,64]{1,0:T(8,128)S(1)}) custom-call(f32[64,128]{1,0:T(8,128)S(1)} %add.66.gram_ref, f32[64,64]{1,0:T(8,128)S(1)} %first.1.inverse_ref, f32[8,128]{1,0:T(8,128)S(1)} %add_multiply_fusion.shift_ref), custom_call_target="tpu_custom_call" | custom-call | tf_op jit(solution)/shard_map/second/pallas_call | solution.py:608
  93.5 1.7 %blend.3 = (f32[16,64,128]{2,1,0:T(8,128)S(1)}, f32[16,64,128]{2,1,0:T(8,128)S(1)}, f32[64,64]{1,0:T(8,128)S(1)}) custom-call(s32[4]{0:T(128)S(1)} %pad_add_fusion.place_ref, f32[32,64,128]{2,1,0:T(8,128)S(1)} %get-tuple-element.119.refs_3_.x_ref, f32[32,32,128]{2,1,0:T(8,128)S(1)} %get-tuple-element.101.x_ref.a_ref, ...), custom_call_target="tpu_custom_call" | custom-call | tf_op jit(solution)/shard_map/blend/pallas_call | solution.py:448
  95.3 1.7 %blend.2 = (f32[16,64,128]{2,1,0:T(8,128)S(1)}, f32[16,64,128]{2,1,0:T(8,128)S(1)}, f32[64,64]{1,0:T(8,128)S(1)}) custom-call(s32[4]{0:T(128)S(1)} %pad_add_fusion.place_ref, f32[32,64,128]{2,1,0:T(8,128)S(1)} %get-tuple-element.119.refs_3_.x_ref, f32[32,32,128]{2,1,0:T(8,128)S(1)} %get-tuple-element.101.x_ref.a_ref, ...), custom_call_target="tpu_custom_call" | custom-call | tf_op jit(solution)/shard_map/blend/pallas_call | solution.py:448
  98.4 1.5 %collective-permute-done.32.other_ref = f32[16,32,128]{2,1,0:T(8,128)S(1)} collective-permute-done((f32[16,32,128]{2,1,0:T(8,128)S(1)}, f32[16,32,128]{2,1,0:T(8,128)S(1)}, u32[]{:S(2)}, u32[]{:S(2)}) %collective-permute-start.32) | collective-permute-done | bytes 262176 | tf_op jit(solution)/shard_map/ppermute | solution.py:614
  100.0 2.0 %third.1 = (f32[32,64,128]{2,1,0:T(8,128)S(1)}, f32[72,128]{1,0:T(8,128)S(1)}) custom-call(s32[4]{0:T(128)S(1)} %pad_add_fusion.place_ref, f32[16,32,128]{2,1,0:T(8,128)S(1)} %add.68.mine_ref, f32[16,32,128]{2,1,0:T(8,128)S(1)} %collective-permute-done.32.other_ref, f32[64,64]{1,0:T(8,128)S(1)} %get-tuple-element.134.gain_ref, ...), custom_call_target="tpu_custom_call" | custom-call | tf_op jit(solution)/shard_map/third/pallas_call | solution.py:615
  102.0 2.4 %collective-permute-start.35 = (f32[72,128]{1,0:T(8,128)S(1)}, f32[72,128]{1,0:T(8,128)S(1)}, u32[]{:S(2)}, u32[]{:S(2)}) collective-permute-start(f32[72,128]{1,0:T(8,128)S(1)} %get-tuple-element.140), channel_id=1, source_target_pairs={{0,12},{4,8},{8,4},{12,0},{1,13},{5,9},{9,5},{13,1},{2,14},{6,10},... | collective-permute-start | bytes 110600 | tf_op jit(solution)/shard_map/ppermute | solution.py:161
  104.4 1.9 %collective-permute-start.34 = (f32[72,128]{1,0:T(8,128)S(1)}, f32[72,128]{1,0:T(8,128)S(1)}, u32[]{:S(2)}, u32[]{:S(2)}) collective-permute-start(f32[72,128]{1,0:T(8,128)S(1)} %get-tuple-element.140), channel_id=1, source_target_pairs={{0,8},{4,12},{8,0},{12,4},{1,9},{5,13},{9,1},{13,5},{2,10},{6,14},... | collective-permute-start | bytes 110600 | tf_op jit(solution)/shard_map/ppermute | solution.py:161
  107.8 1.6 %collective-permute-done.34 = f32[72,128]{1,0:T(8,128)S(1)} collective-permute-done((f32[72,128]{1,0:T(8,128)S(1)}, f32[72,128]{1,0:T(8,128)S(1)}, u32[]{:S(2)}, u32[]{:S(2)}) %collective-permute-start.34) | collective-permute-done | bytes 36896 | tf_op jit(solution)/shard_map/ppermute | solution.py:161
  110.3 3.1 %fourth.1 = (f32[64,64]{1,0:T(8,128)S(1)}, f32[64,64]{1,0:T(8,128)S(1)}, f32[64,128]{1,0:T(8,128)S(1)}) custom-call(f32[72,128]{1,0:T(8,128)S(1)} %add_add_fusion.gram_ref, f32[8,128]{1,0:T(8,128)S(1)} %add_multiply_fusion.shift_ref), custom_call_target="tpu_custom_call" | custom-call | tf_op jit(solution)/shard_map/fourth/pallas_call | solution.py:623
  113.4 1.9 %last.1 = (f32[32,64,128]{2,1,0:T(8,128)}, f32[4,64,64]{2,1,0:T(8,128)}) custom-call(f32[32,64,128]{2,1,0:T(8,128)S(1)} %get-tuple-element.139.w_ref, f32[16,64,128]{2,1,0:T(8,128)S(1)} %get-tuple-element.137.refs_2_.low_ref, f32[16,64,128]{2,1,0:T(8,128)S(1)} %get-tuple-element.138.refs_3_.high_ref, f32[64,128]{1,0:T(8,128)S(1)} %get-tuple-element.141.coef_ref, ...), custom_call_target="tpu_custom_call" | custom-call | tf_op jit(solution)/shard_map/last/pallas_call | solution.py:626
  (98 shorter events, 35.6 us)
Async XLA Ops:
  0.6 17.0 %collective-permute-start.2 = (s32[1,1,44]{2,1,0:T(1,128)}, s32[1,1,44]{2,1,0:T(1,128)S(1)}, u32[]{:S(2)}, u32[]{:S(2)}) collective-permute-start(s32[1,1,44]{2,1,0:T(1,128)} %cols_ref.5), channel_id=1, source_target_pairs={{4,8},{0,12},{8,4},{12,0},{5,9},{1,13},{9,5},{13,1},{6,10},{2,14},... | collective-permute-start | bytes 536 | tf_op jit(solution)/shard_map/ppermute | solution.py:119
  5.8 11.9 %collective-permute-start.1 = (s32[1,1,44]{2,1,0:T(1,128)}, s32[1,1,44]{2,1,0:T(1,128)S(1)}, u32[]{:S(2)}, u32[]{:S(2)}) collective-permute-start(s32[1,1,44]{2,1,0:T(1,128)} %cols_ref.5), channel_id=1, source_target_pairs={{0,4},{8,12},{4,0},{12,8},{1,5},{9,13},{5,1},{13,9},{2,6},{10,14},... | collective-permute-start | bytes 536 | tf_op jit(solution)/shard_map/ppermute | solution.py:119
  5.8 12.0 %collective-permute-start = (s32[1,1,44]{2,1,0:T(1,128)}, s32[1,1,44]{2,1,0:T(1,128)S(1)}, u32[]{:S(2)}, u32[]{:S(2)}) collective-permute-start(s32[1,1,44]{2,1,0:T(1,128)} %cols_ref.5), channel_id=1, source_target_pairs={{0,8},{4,12},{8,0},{12,4},{1,9},{5,13},{9,1},{13,5},{2,10},{6,14},... | collective-permute-start | bytes 536 | tf_op jit(solution)/shard_map/ppermute | solution.py:119
  8.4 3.7 %collective-permute-start.6 = (f32[8,128]{1,0:T(8,128)S(1)}, f32[8,128]{1,0:T(8,128)S(1)}, u32[]{:S(2)}, u32[]{:S(2)}) collective-permute-start(f32[8,128]{1,0:T(8,128)S(1)} %broadcast_in_dim.8), channel_id=1, source_target_pairs={{0,4},{4,0},{8,12},{12,8},{1,5},{5,1},{9,13},{13,9},{2,6},{6,2},{1... | collective-permute-start | bytes 12296 | tf_op jit(solution)/shard_map/ppermute | solution.py:140
  12.1 11.3 %collective-permute-start.7 = (f32[8,128]{1,0:T(8,128)S(1)}, f32[8,128]{1,0:T(8,128)S(1)}, u32[]{:S(2)}, u32[]{:S(2)}) collective-permute-start(f32[8,128]{1,0:T(8,128)S(1)} %broadcast_add_fusion), channel_id=1, source_target_pairs={{0,8},{4,12},{8,0},{12,4},{1,9},{5,13},{9,1},{13,5},{2,10},{6,14},... | collective-permute-start | bytes 12296 | tf_op jit(solution)/shard_map/ppermute | solution.py:149
  19.2 16.9 %collective-permute-start.3 = (f32[8,32,128]{2,1,0:T(8,128)S(1)}, f32[8,32,128]{2,1,0:T(8,128)S(1)}, u32[]{:S(2)}, u32[]{:S(2)}) collective-permute-start(f32[8,32,128]{2,1,0:T(8,128)S(1)} %get-tuple-element.77), channel_id=1, source_target_pairs={{0,8},{4,12},{8,0},{12,4},{1,9},{5,13},{9,1},{13,5},{2,10},{6,14},... | collective-permute-start | bytes 393224 | tf_op jit(solution)/shard_map/ppermute | solution.py:119
  19.4 12.7 %collective-permute-start.4 = (f32[8,32,128]{2,1,0:T(8,128)S(1)}, f32[8,32,128]{2,1,0:T(8,128)S(1)}, u32[]{:S(2)}, u32[]{:S(2)}) collective-permute-start(f32[8,32,128]{2,1,0:T(8,128)S(1)} %get-tuple-element.78), channel_id=1, source_target_pairs={{4,8},{0,12},{8,4},{12,0},{5,9},{1,13},{9,5},{13,1},{6,10},{2,14},... | collective-permute-start | bytes 393224 | tf_op jit(solution)/shard_map/ppermute | solution.py:119
  23.4 7.1 %collective-permute-start.5 = (f32[8,32,128]{2,1,0:T(8,128)S(1)}, f32[8,32,128]{2,1,0:T(8,128)S(1)}, u32[]{:S(2)}, u32[]{:S(2)}) collective-permute-start(f32[8,32,128]{2,1,0:T(8,128)S(1)} %get-tuple-element.79), channel_id=1, source_target_pairs={{0,4},{8,12},{4,0},{12,8},{1,5},{9,13},{5,1},{13,9},{2,6},{10,14},... | collective-permute-start | bytes 393224 | tf_op jit(solution)/shard_map/ppermute | solution.py:119
  32.0 4.0 %collective-permute-start.8 = (f32[64,64]{1,0:T(8,128)S(1)}, f32[64,64]{1,0:T(8,128)S(1)}, u32[]{:S(2)}, u32[]{:S(2)}) collective-permute-start(f32[64,64]{1,0:T(8,128)S(1)} %gram.1), channel_id=1, source_target_pairs={{0,4},{4,0},{8,12},{12,8},{1,5},{5,1},{9,13},{13,9},{2,6},{6,2},{1... | collective-permute-start | bytes 49160 | tf_op jit(solution)/shard_map/ppermute | solution.py:140
  33.0 8.0 %collective-permute-start.11 = (f32[8,32,128]{2,1,0:T(8,128)S(1)}, f32[8,32,128]{2,1,0:T(8,128)S(1)}, u32[]{:S(2)}, u32[]{:S(2)}) collective-permute-start(f32[8,32,128]{2,1,0:T(8,128)S(1)} %get-tuple-element.91), channel_id=1, source_target_pairs={{0,4},{8,12},{4,0},{12,8},{1,5},{9,13},{5,1},{13,9},{2,6},{10,14},... | collective-permute-start | bytes 393224 | tf_op jit(solution)/shard_map/ppermute | solution.py:119
  36.0 8.2 %collective-permute-start.12 = (f32[64,64]{1,0:T(8,128)S(1)}, f32[64,64]{1,0:T(8,128)S(1)}, u32[]{:S(2)}, u32[]{:S(2)}) collective-permute-start(f32[64,64]{1,0:T(8,128)S(1)} %add.57), channel_id=1, source_target_pairs={{0,8},{4,12},{8,0},{12,4},{1,9},{5,13},{9,1},{13,5},{2,10},{6,14},... | collective-permute-start | bytes 49160 | tf_op jit(solution)/shard_map/ppermute | solution.py:149
  37.1 14.1 %collective-permute-start.9 = (f32[8,32,128]{2,1,0:T(8,128)S(1)}, f32[8,32,128]{2,1,0:T(8,128)S(1)}, u32[]{:S(2)}, u32[]{:S(2)}) collective-permute-start(f32[8,32,128]{2,1,0:T(8,128)S(1)} %get-tuple-element.88), channel_id=1, source_target_pairs={{0,8},{4,12},{8,0},{12,4},{1,9},{5,13},{9,1},{13,5},{2,10},{6,14},... | collective-permute-start | bytes 393224 | tf_op jit(solution)/shard_map/ppermute | solution.py:119
  39.7 6.9 %collective-permute-start.10 = (f32[8,32,128]{2,1,0:T(8,128)S(1)}, f32[8,32,128]{2,1,0:T(8,128)S(1)}, u32[]{:S(2)}, u32[]{:S(2)}) collective-permute-start(f32[8,32,128]{2,1,0:T(8,128)S(1)} %get-tuple-element.90), channel_id=1, source_target_pairs={{4,8},{0,12},{8,4},{12,0},{5,9},{1,13},{9,5},{13,1},{6,10},{2,14},... | collective-permute-start | bytes 393224 | tf_op jit(solution)/shard_map/ppermute | solution.py:119
  42.6 8.4 %collective-permute-start.15 = (f32[16,32,128]{2,1,0:T(8,128)S(1)}, f32[16,32,128]{2,1,0:T(8,128)S(1)}, u32[]{:S(2)}, u32[]{:S(2)}) collective-permute-start(f32[16,32,128]{2,1,0:T(8,128)S(1)} %add.58), channel_id=1, source_target_pairs={{0,2},{1,3},{2,0},{3,1},{4,6},{5,7},{6,4},{7,5},{8,10},{9,11},{10,... | collective-permute-start | bytes 786440 | tf_op jit(solution)/shard_map/ppermute | solution.py:514
  54.3 8.3 %collective-permute-start.17 = (f32[16,32,128]{2,1,0:T(8,128)S(1)}, f32[16,32,128]{2,1,0:T(8,128)S(1)}, u32[]{:S(2)}, u32[]{:S(2)}) collective-permute-start(f32[16,32,128]{2,1,0:T(8,128)S(1)} %add.61), channel_id=1, source_target_pairs={{0,2},{1,3},{2,0},{3,1},{4,6},{5,7},{6,4},{7,5},{8,10},{9,11},{10,... | collective-permute-start | bytes 786440 | tf_op jit(solution)/shard_map/ppermute | solution.py:514
  55.8 9.0 %collective-permute-start.19 = (f32[8,32,128]{2,1,0:T(8,128)S(1)}, f32[8,32,128]{2,1,0:T(8,128)S(1)}, u32[]{:S(2)}, u32[]{:S(2)}) collective-permute-start(f32[8,32,128]{2,1,0:T(8,128)S(1)} %get-tuple-element.106), channel_id=1, source_target_pairs={{0,8},{4,12},{8,0},{12,4},{1,9},{5,13},{9,1},{13,5},{2,10},{6,14},... | collective-permute-start | bytes 393224 | tf_op jit(solution)/shard_map/ppermute | solution.py:119
  57.5 11.5 %collective-permute-start.23 = (f32[8,32,128]{2,1,0:T(8,128)S(1)}, f32[8,32,128]{2,1,0:T(8,128)S(1)}, u32[]{:S(2)}, u32[]{:S(2)}) collective-permute-start(f32[8,32,128]{2,1,0:T(8,128)S(1)} %get-tuple-element.113), channel_id=1, source_target_pairs={{0,4},{8,12},{4,0},{12,8},{1,5},{9,13},{5,1},{13,9},{2,6},{10,14},... | collective-permute-start | bytes 393224 | tf_op jit(solution)/shard_map/ppermute | solution.py:119
  60.0 7.8 %collective-permute-start.24 = (f32[8,32,128]{2,1,0:T(8,128)S(1)}, f32[8,32,128]{2,1,0:T(8,128)S(1)}, u32[]{:S(2)}, u32[]{:S(2)}) collective-permute-start(f32[8,32,128]{2,1,0:T(8,128)S(1)} %get-tuple-element.114), channel_id=1, source_target_pairs={{4,8},{0,12},{8,4},{12,0},{5,9},{1,13},{9,5},{13,1},{6,10},{2,14},... | collective-permute-start | bytes 393224 | tf_op jit(solution)/shard_map/ppermute | solution.py:119
  62.7 3.1 %collective-permute-start.18 = (f32[16,32,128]{2,1,0:T(8,128)S(1)}, f32[16,32,128]{2,1,0:T(8,128)S(1)}, u32[]{:S(2)}, u32[]{:S(2)}) collective-permute-start(f32[16,32,128]{2,1,0:T(8,128)S(1)} %add.62.refs_3_), channel_id=1, source_target_pairs={{0,1},{1,0},{2,3},{3,2},{4,5},{5,4},{6,7},{7,6},{8,9},{9,8},{10,11... | collective-permute-start | bytes 786440 | tf_op jit(solution)/shard_map/ppermute | solution.py:588
  67.2 9.2 %collective-permute-start.22 = (f32[8,32,128]{2,1,0:T(8,128)S(1)}, f32[8,32,128]{2,1,0:T(8,128)S(1)}, u32[]{:S(2)}, u32[]{:S(2)}) collective-permute-start(f32[8,32,128]{2,1,0:T(8,128)S(1)} %get-tuple-element.111), channel_id=1, source_target_pairs={{0,4},{8,12},{4,0},{12,8},{1,5},{9,13},{5,1},{13,9},{2,6},{10,14},... | collective-permute-start | bytes 393224 | tf_op jit(solution)/shard_map/ppermute | solution.py:119
  70.2 13.0 %collective-permute-start.20 = (f32[8,32,128]{2,1,0:T(8,128)S(1)}, f32[8,32,128]{2,1,0:T(8,128)S(1)}, u32[]{:S(2)}, u32[]{:S(2)}) collective-permute-start(f32[8,32,128]{2,1,0:T(8,128)S(1)} %get-tuple-element.109), channel_id=1, source_target_pairs={{0,8},{4,12},{8,0},{12,4},{1,9},{5,13},{9,1},{13,5},{2,10},{6,14},... | collective-permute-start | bytes 393224 | tf_op jit(solution)/shard_map/ppermute | solution.py:119
  72.5 8.5 %collective-permute-start.21 = (f32[8,32,128]{2,1,0:T(8,128)S(1)}, f32[8,32,128]{2,1,0:T(8,128)S(1)}, u32[]{:S(2)}, u32[]{:S(2)}) collective-permute-start(f32[8,32,128]{2,1,0:T(8,128)S(1)} %get-tuple-element.110), channel_id=1, source_target_pairs={{4,8},{0,12},{8,4},{12,0},{5,9},{1,13},{9,5},{13,1},{6,10},{2,14},... | collective-permute-start | bytes 393224 | tf_op jit(solution)/shard_map/ppermute | solution.py:119
  74.7 2.7 %collective-permute-start.25 = (f32[16,32,128]{2,1,0:T(8,128)S(1)}, f32[16,32,128]{2,1,0:T(8,128)S(1)}, u32[]{:S(2)}, u32[]{:S(2)}) collective-permute-start(f32[16,32,128]{2,1,0:T(8,128)S(1)} %get-tuple-element.120), channel_id=1, source_target_pairs={{0,1},{1,0},{2,3},{3,2},{4,5},{5,4},{6,7},{7,6},{8,9},{9,8},{10,11... | collective-permute-start | bytes 786440 | tf_op jit(solution)/shard_map/ppermute | solution.py:594
  78.5 4.6 %collective-permute-start.26 = (f32[64,128]{1,0:T(8,128)S(1)}, f32[64,128]{1,0:T(8,128)S(1)}, u32[]{:S(2)}, u32[]{:S(2)}) collective-permute-start(f32[64,128]{1,0:T(8,128)S(1)} %cross.1), channel_id=1, source_target_pairs={{0,4},{4,0},{8,12},{12,8},{1,5},{5,1},{9,13},{13,9},{2,6},{6,2},{1... | collective-permute-start | bytes 98312 | tf_op jit(solution)/shard_map/ppermute | solution.py:140
  78.6 10.8 %collective-permute-start.28 = (f32[16,32,128]{2,1,0:T(8,128)S(1)}, f32[16,32,128]{2,1,0:T(8,128)S(1)}, u32[]{:S(2)}, u32[]{:S(2)}) collective-permute-start(f32[16,32,128]{2,1,0:T(8,128)S(1)} %add.63), channel_id=1, source_target_pairs={{0,2},{1,3},{2,0},{3,1},{4,6},{5,7},{6,4},{7,5},{8,10},{9,11},{10,... | collective-permute-start | bytes 786440 | tf_op jit(solution)/shard_map/ppermute | solution.py:514
  84.2 5.3 %collective-permute-start.27 = (f32[16,32,128]{2,1,0:T(8,128)S(1)}, f32[16,32,128]{2,1,0:T(8,128)S(1)}, u32[]{:S(2)}, u32[]{:S(2)}) collective-permute-start(f32[16,32,128]{2,1,0:T(8,128)S(1)} %get-tuple-element.126), channel_id=1, source_target_pairs={{0,1},{1,0},{2,3},{3,2},{4,5},{5,4},{6,7},{7,6},{8,9},{9,8},{10,11... | collective-permute-start | bytes 786440 | tf_op jit(solution)/shard_map/ppermute | solution.py:603
  84.3 5.1 %collective-permute-start.29 = (f32[64,128]{1,0:T(8,128)S(1)}, f32[64,128]{1,0:T(8,128)S(1)}, u32[]{:S(2)}, u32[]{:S(2)}) collective-permute-start(f32[64,128]{1,0:T(8,128)S(1)} %add.64), channel_id=1, source_target_pairs={{0,8},{4,12},{8,0},{12,4},{1,9},{5,13},{9,1},{13,5},{2,10},{6,14},... | collective-permute-start | bytes 98312 | tf_op jit(solution)/shard_map/ppermute | solution.py:149
  89.4 4.1 %collective-permute-start.31 = (f32[16,32,128]{2,1,0:T(8,128)S(1)}, f32[16,32,128]{2,1,0:T(8,128)S(1)}, u32[]{:S(2)}, u32[]{:S(2)}) collective-permute-start(f32[16,32,128]{2,1,0:T(8,128)S(1)} %add.65.mine_ref), channel_id=1, source_target_pairs={{0,1},{1,0},{2,3},{3,2},{4,5},{5,4},{6,7},{7,6},{8,9},{9,8},{10,11... | collective-permute-start | bytes 786440 | tf_op jit(solution)/shard_map/ppermute | solution.py:605
  89.5 8.8 %collective-permute-start.30 = (f32[16,32,128]{2,1,0:T(8,128)S(1)}, f32[16,32,128]{2,1,0:T(8,128)S(1)}, u32[]{:S(2)}, u32[]{:S(2)}) collective-permute-start(f32[16,32,128]{2,1,0:T(8,128)S(1)} %add.67), channel_id=1, source_target_pairs={{0,2},{1,3},{2,0},{3,1},{4,6},{5,7},{6,4},{7,5},{8,10},{9,11},{10,... | collective-permute-start | bytes 786440 | tf_op jit(solution)/shard_map/ppermute | solution.py:514
  102.0 5.8 %collective-permute-start.35 = (f32[72,128]{1,0:T(8,128)S(1)}, f32[72,128]{1,0:T(8,128)S(1)}, u32[]{:S(2)}, u32[]{:S(2)}) collective-permute-start(f32[72,128]{1,0:T(8,128)S(1)} %get-tuple-element.140), channel_id=1, source_target_pairs={{0,12},{4,8},{8,4},{12,0},{1,13},{5,9},{9,5},{13,1},{2,14},{6,10},... | collective-permute-start | bytes 110600 | tf_op jit(solution)/shard_map/ppermute | solution.py:161
  104.4 5.1 %collective-permute-start.34 = (f32[72,128]{1,0:T(8,128)S(1)}, f32[72,128]{1,0:T(8,128)S(1)}, u32[]{:S(2)}, u32[]{:S(2)}) collective-permute-start(f32[72,128]{1,0:T(8,128)S(1)} %get-tuple-element.140), channel_id=1, source_target_pairs={{0,8},{4,12},{8,0},{12,4},{1,9},{5,13},{9,1},{13,5},{2,10},{6,14},... | collective-permute-start | bytes 110600 | tf_op jit(solution)/shard_map/ppermute | solution.py:161
  106.3 4.0 %collective-permute-start.33 = (f32[72,128]{1,0:T(8,128)S(1)}, f32[72,128]{1,0:T(8,128)S(1)}, u32[]{:S(2)}, u32[]{:S(2)}) collective-permute-start(f32[72,128]{1,0:T(8,128)S(1)} %get-tuple-element.140), channel_id=1, source_target_pairs={{0,4},{4,0},{8,12},{12,8},{1,5},{5,1},{9,13},{13,9},{2,6},{6,2},{1... | collective-permute-start | bytes 110600 | tf_op jit(solution)/shard_map/ppermute | solution.py:161
  (8 other events, 52.6 us)
